TPU v7x, 32 devices: a whole 2x2x4 slice. The times are simulated.
32 devices in a mesh: seq: 4 (over y, x), batch: 8 (over z, core).
Axes of the slice: x: 2, y: 2, z: 4, core: 2. Of those that a mesh axis runs over, the one named last changes fastest.
Arguments:
- layer_input: bfloat16 [8, 1024, 2048], P('batch', 'seq'), may hold values from -6 to 6
- segments: int32 [8, 1024], P('batch', 'seq'), may hold values from 0 to 128, as said below
- mixer_gain: bfloat16 [2048], P(('seq', 'batch')), may hold values from 0.5 to 1.5
- query_weight: bfloat16 [2048, 2048], P(('seq', 'batch')), may hold values from -0.125 to 0.125
- key_weight: bfloat16 [2048, 2048], P(('seq', 'batch')), may hold values from -0.125 to 0.125
- value_weight: bfloat16 [2048, 2048], P(('seq', 'batch')), may hold values from -0.125 to 0.125
- squeeze: bfloat16 [2048, 16], P(('seq', 'batch')), may hold values from -0.125 to 0.125
- expand: bfloat16 [16, 256], P(None, ('seq', 'batch')), may hold values from -1.5 to 1.5
- forget_bias: bfloat16 [256], P(('seq', 'batch')), may hold values from 1 to 9
- swish_weight: bfloat16 [2048, 2048], P(('seq', 'batch')), may hold values from -0.125 to 0.125
- head_gain: bfloat16 [2048], P(('seq', 'batch')), may hold values from 0.5 to 1.5
- output_weight: bfloat16 [2048, 2048], P(('seq', 'batch')), may hold values from -0.125 to 0.125
- feed_gain: bfloat16 [2048], P(('seq', 'batch')), may hold values from 0.5 to 1.5
- gate_weight: bfloat16 [2048, 5632], P(('seq', 'batch')), may hold values from -0.125 to 0.125
- up_weight: bfloat16 [2048, 5632], P(('seq', 'batch')), may hold values from -0.125 to 0.125
- down_weight: bfloat16 [5632, 2048], P(('seq', 'batch')), may hold values from -0.078125 to 0.078125
- cotangent: bfloat16 [8, 1024, 2048], P('batch', 'seq'), may hold values from -6 to 6
Outputs:
- layer_output: bfloat16 [8, 1024, 2048], P('batch', 'seq')
- grad_input: bfloat16 [8, 1024, 2048], P('batch', 'seq')
- grad_mixer: float32 [2048], P(('seq', 'batch'))
- grad_query: float32 [2048, 2048], P(('seq', 'batch'))
- grad_key: float32 [2048, 2048], P(('seq', 'batch'))
- grad_value: float32 [2048, 2048], P(('seq', 'batch'))
- grad_squeeze: float32 [2048, 16], P(('seq', 'batch'))
- grad_expand: float32 [16, 256], P(None, ('seq', 'batch'))
- grad_bias: float32 [256], P(('seq', 'batch'))
- grad_swish: float32 [2048, 2048], P(('seq', 'batch'))
- grad_head: float32 [2048], P(('seq', 'batch'))
- grad_output: float32 [2048, 2048], P(('seq', 'batch'))
- grad_feed: float32 [2048], P(('seq', 'batch'))
- grad_gate: float32 [2048, 5632], P(('seq', 'batch'))
- grad_up: float32 [2048, 5632], P(('seq', 'batch'))
- grad_down: float32 [5632, 2048], P(('seq', 'batch'))
Inputs may be any that keep to these rules, and one draw needn't show every extreme that they name: `segments`: document numbers start at 0 in each sequence, never fall and rise by one where a document starts; each sequence holds exactly 129 documents. In every sequence one document begins within the first 128 positions and ends within the last 128; all other documents lie there too.
All inputs are finite; a program needn't handle non-finite values.
Results may differ from a plain program's by a relative error of at most 0.025.
Values may be sent and summed in bfloat16 or wider, within the bound.
A program may use at most 512 MiB of HBM per device.

v0:
```python
import jax
import jax.numpy as jnp
from jax import lax
from jax.sharding import PartitionSpec as P

HEADS = 4
SLOTS = 64


EPS = 1e-06
TAU_GATE = 8.0


def shifted(shard, axis, by):
    length = lax.axis_size(axis)
    pairs = [(i, i + by) for i in range(length) if 0 <= i + by < length]
    return lax.ppermute(shard, axis, pairs)


def highest(left, right):
    return jnp.dot(left, right, precision=lax.Precision.HIGHEST, preferred_element_type=jnp.float32)


def rms_scale(features):
    return lax.rsqrt(jnp.mean(features * features, axis=-1, keepdims=True) + EPS)


def silu_slope(preact):
    sigma = jax.nn.sigmoid(preact)
    return sigma * (1.0 + preact * (1.0 - sigma))


def head_output(
    query_rows, key_rows, value_rows, log_rate, segment, last_prev, key_state, value_state
):
    positions = jnp.arange(query_rows.shape[0])
    factor = query_rows.shape[1] ** (-0.25)
    cumulative = jnp.cumsum(log_rate, axis=0)
    inflow = -jnp.expm1(log_rate)
    visible = (segment[:, None] == segment[None, :]) & (positions[None, :] <= positions[:, None])
    spread = jnp.where(visible[:, :, None], cumulative[:, None, :] - cumulative[None, :, :], 0.0)
    weight = jnp.exp(spread) * visible.astype(jnp.float32)[:, :, None] * inflow[None, :, :]
    carried = (segment == last_prev).astype(jnp.float32)[:, None] * jnp.exp(cumulative)
    scores = highest(query_rows, key_rows.T) * factor
    logits = jnp.einsum("tsm,ts->tm", weight, scores, precision=lax.Precision.HIGHEST)
    logits = logits + carried * highest(query_rows, key_state.T) * factor
    attention = jax.nn.softmax(logits, axis=-1)
    mixing = jnp.einsum("tm,tsm->ts", attention, weight, precision=lax.Precision.HIGHEST)
    return highest(mixing, value_rows) + highest(attention * carried, value_state)


def head_end(key_rows, value_rows, log_rate, segment, last_prev, key_state, value_state):
    cumulative = jnp.cumsum(log_rate, axis=0)
    inflow = -jnp.expm1(log_rate)
    visible = segment == segment[-1]
    spread = jnp.where(visible[:, None], cumulative[-1][None, :] - cumulative, 0.0)
    weight = jnp.exp(spread) * visible.astype(jnp.float32)[:, None] * inflow
    carried_end = (segment[-1] == last_prev).astype(jnp.float32) * jnp.exp(cumulative[-1])
    key_end = highest(weight.T, key_rows) + carried_end[:, None] * key_state
    value_end = highest(weight.T, value_rows) + carried_end[:, None] * value_state
    return (key_end, value_end)


def mixer_heads(query_h, key_h, value_h, rate_h, segment, last_prev, key_state, value_state):

    def mixer_one_head(per_head):
        return head_output(
            per_head[0],
            per_head[1],
            per_head[2],
            per_head[3],
            segment,
            last_prev,
            per_head[4],
            per_head[5],
        )

    return lax.map(
        jax.checkpoint(mixer_one_head), (query_h, key_h, value_h, rate_h, key_state, value_state)
    )


def ends_heads(key_h, value_h, rate_h, segment, last_prev, key_state, value_state):

    def ends_one_head(per_head):
        return head_end(
            per_head[0], per_head[1], per_head[2], segment, last_prev, per_head[3], per_head[4]
        )

    return lax.map(ends_one_head, (key_h, value_h, rate_h, key_state, value_state))


def local(
    layer_input,
    segments,
    mixer_gain,
    query_weight,
    key_weight,
    value_weight,
    squeeze,
    expand,
    forget_bias,
    swish_weight,
    head_gain,
    output_weight,
    feed_gain,
    gate_weight,
    up_weight,
    down_weight,
    cotangent,
):
    row_count = layer_input.shape[1]
    model_width = layer_input.shape[2]
    head_size = model_width // HEADS

    def to_heads(rows_in, inner):
        return rows_in.reshape(row_count, HEADS, inner).transpose(1, 0, 2)

    def from_heads(heads_in):
        return heads_in.transpose(1, 0, 2).reshape(row_count, -1)

    mixer_parts = (
        lax.all_gather(query_weight, ("seq", "batch"), axis=0, tiled=True),
        lax.all_gather(key_weight, ("seq", "batch"), axis=0, tiled=True),
        lax.all_gather(value_weight, ("seq", "batch"), axis=0, tiled=True),
        lax.all_gather(swish_weight, ("seq", "batch"), axis=0, tiled=True),
        lax.all_gather(output_weight, ("seq", "batch"), axis=0, tiled=True),
        lax.all_gather(squeeze, ("seq", "batch"), axis=0, tiled=True),
        lax.all_gather(expand, ("seq", "batch"), axis=1, tiled=True),
        lax.all_gather(forget_bias, ("seq", "batch"), axis=0, tiled=True),
        lax.all_gather(mixer_gain, ("seq", "batch"), axis=0, tiled=True),
        lax.all_gather(head_gain, ("seq", "batch"), axis=0, tiled=True),
    )
    (
        w_query,
        w_key,
        w_value,
        w_swish,
        w_output,
        w_squeeze,
        w_expand,
        bias_full,
        gain_one,
        gain_head,
    ) = mixer_parts
    inputs_f = layer_input.reshape(row_count, model_width).astype(jnp.float32)
    segment = segments.reshape(row_count).astype(jnp.float32)
    scale_one = rms_scale(inputs_f)
    gain_onef = gain_one.astype(jnp.float32)
    normed = (inputs_f * scale_one * gain_onef).astype(jnp.bfloat16)
    query_rows = jnp.dot(normed, w_query, preferred_element_type=jnp.float32).astype(jnp.bfloat16)
    key_rows = jnp.dot(normed, w_key, preferred_element_type=jnp.float32).astype(jnp.bfloat16)
    value_rows = jnp.dot(normed, w_value, preferred_element_type=jnp.float32).astype(jnp.bfloat16)
    reduced = jnp.dot(normed, w_squeeze, preferred_element_type=jnp.float32).astype(jnp.bfloat16)
    forget_logit = jnp.dot(
        reduced, w_expand, preferred_element_type=jnp.float32
    ) + bias_full.astype(jnp.float32)
    log_rate = jax.nn.log_sigmoid(forget_logit) / TAU_GATE
    swish_pre = jnp.dot(normed, w_swish, preferred_element_type=jnp.float32)
    query_h = to_heads(query_rows.astype(jnp.float32), head_size)
    key_h = to_heads(key_rows.astype(jnp.float32), head_size)
    value_h = to_heads(value_rows.astype(jnp.float32), head_size)
    rate_h = to_heads(log_rate, SLOTS)
    zero_state = jnp.zeros((HEADS, SLOTS, head_size), jnp.float32)
    key_local, value_local = ends_heads(
        key_h, value_h, rate_h, segment, jnp.float32(-1.0), zero_state, zero_state
    )
    through = jnp.exp(jnp.cumsum(rate_h, axis=1)[:, -1, :])
    last_seg = segment[-1:]
    key_init = zero_state
    value_init = zero_state
    last_held = jnp.zeros((1,), jnp.float32)
    for rounds in range(lax.axis_size("seq") - 1):
        passing = (segment[-1] == last_held[0]).astype(jnp.float32) * through
        key_init, value_init, last_held = shifted(
            (
                passing[..., None] * key_init + key_local,
                passing[..., None] * value_init + value_local,
                last_seg,
            ),
            "seq",
            1,
        )
    last_prev = last_held[0]
    mixed_h = mixer_heads(query_h, key_h, value_h, rate_h, segment, last_prev, key_init, value_init)
    per_head = mixed_h.transpose(1, 0, 2)
    head_factor = rms_scale(per_head)
    gain_headf = gain_head.astype(jnp.float32)
    head_plain = (per_head * head_factor).reshape(row_count, model_width)
    head_normed = head_plain * gain_headf
    swish_act = jax.nn.silu(swish_pre)
    gated = (head_normed * swish_act).astype(jnp.bfloat16)
    hidden = inputs_f + jnp.dot(gated, w_output, preferred_element_type=jnp.float32)
    feed_parts = (
        lax.all_gather(gate_weight, ("seq", "batch"), axis=0, tiled=True),
        lax.all_gather(up_weight, ("seq", "batch"), axis=0, tiled=True),
        lax.all_gather(down_weight, ("seq", "batch"), axis=0, tiled=True),
        lax.all_gather(feed_gain, ("seq", "batch"), axis=0, tiled=True),
    )
    w_gate, w_up, w_down, gain_two = feed_parts
    scale_two = rms_scale(hidden)
    gain_twof = gain_two.astype(jnp.float32)
    feed_in = (hidden * scale_two * gain_twof).astype(jnp.bfloat16)
    gate_pre = jnp.dot(feed_in, w_gate, preferred_element_type=jnp.float32)
    up_pre = jnp.dot(feed_in, w_up, preferred_element_type=jnp.float32)
    gate_act = jax.nn.silu(gate_pre)
    inner = (gate_act * up_pre).astype(jnp.bfloat16)
    result = hidden + jnp.dot(inner, w_down, preferred_element_type=jnp.float32)
    layer_output = result.astype(jnp.bfloat16).reshape(1, row_count, model_width)
    w_gate, w_up, w_down, gain_two = (
        lax.all_gather(gate_weight, ("seq", "batch"), axis=0, tiled=True),
        lax.all_gather(up_weight, ("seq", "batch"), axis=0, tiled=True),
        lax.all_gather(down_weight, ("seq", "batch"), axis=0, tiled=True),
        lax.all_gather(feed_gain, ("seq", "batch"), axis=0, tiled=True),
    )
    gain_twof = gain_two.astype(jnp.float32)
    grad_out = cotangent.reshape(row_count, model_width)
    grad_outf = grad_out.astype(jnp.float32)
    term_down = jnp.einsum("tf,td->fd", inner, grad_out, preferred_element_type=jnp.float32)
    grad_inner = jnp.einsum("td,fd->tf", grad_out, w_down, preferred_element_type=jnp.float32)
    grad_gatepre = (grad_inner * up_pre * silu_slope(gate_pre)).astype(jnp.bfloat16)
    grad_uppre = (grad_inner * gate_act).astype(jnp.bfloat16)
    term_gate = jnp.einsum("td,tf->df", feed_in, grad_gatepre, preferred_element_type=jnp.float32)
    term_up = jnp.einsum("td,tf->df", feed_in, grad_uppre, preferred_element_type=jnp.float32)
    grad_feedin = jnp.einsum(
        "tf,df->td", grad_gatepre, w_gate, preferred_element_type=jnp.float32
    ) + jnp.einsum("tf,df->td", grad_uppre, w_up, preferred_element_type=jnp.float32)
    term_feed = jnp.sum(grad_feedin * hidden * scale_two, axis=0)
    scaled_two = grad_feedin * gain_twof
    grad_hidden = (
        grad_outf
        + scale_two * scaled_two
        - hidden * scale_two**3 * jnp.mean(scaled_two * hidden, axis=-1, keepdims=True)
    )
    feed_grads = (
        lax.psum_scatter(term_gate, ("seq", "batch"), scatter_dimension=0, tiled=True),
        lax.psum_scatter(term_up, ("seq", "batch"), scatter_dimension=0, tiled=True),
        lax.psum_scatter(term_down, ("seq", "batch"), scatter_dimension=0, tiled=True),
        lax.psum_scatter(term_feed, ("seq", "batch"), scatter_dimension=0, tiled=True),
    )
    gate_share, up_share, down_share, feed_share = feed_grads
    mixer_parts = (
        lax.all_gather(query_weight, ("seq", "batch"), axis=0, tiled=True),
        lax.all_gather(key_weight, ("seq", "batch"), axis=0, tiled=True),
        lax.all_gather(value_weight, ("seq", "batch"), axis=0, tiled=True),
        lax.all_gather(swish_weight, ("seq", "batch"), axis=0, tiled=True),
        lax.all_gather(output_weight, ("seq", "batch"), axis=0, tiled=True),
        lax.all_gather(squeeze, ("seq", "batch"), axis=0, tiled=True),
        lax.all_gather(expand, ("seq", "batch"), axis=1, tiled=True),
        lax.all_gather(forget_bias, ("seq", "batch"), axis=0, tiled=True),
        lax.all_gather(mixer_gain, ("seq", "batch"), axis=0, tiled=True),
        lax.all_gather(head_gain, ("seq", "batch"), axis=0, tiled=True),
    )
    (
        w_query,
        w_key,
        w_value,
        w_swish,
        w_output,
        w_squeeze,
        w_expand,
        bias_full,
        gain_one,
        gain_head,
    ) = mixer_parts
    gain_onef = gain_one.astype(jnp.float32)
    gain_headf = gain_head.astype(jnp.float32)
    grad_branch = grad_hidden.astype(jnp.bfloat16)
    grad_gated = jnp.einsum("te,de->td", grad_branch, w_output, preferred_element_type=jnp.float32)
    grad_swishpre = (grad_gated * head_normed * silu_slope(swish_pre)).astype(jnp.bfloat16)
    grad_normed_head = grad_gated * swish_act
    term_head = jnp.sum(grad_normed_head * head_plain, axis=0)
    scaled_head = (grad_normed_head * gain_headf).reshape(row_count, HEADS, head_size)
    grad_mixed = head_factor * scaled_head - per_head * head_factor**3 * jnp.mean(
        scaled_head * per_head, axis=-1, keepdims=True
    )
    grad_mixed_h = grad_mixed.transpose(1, 0, 2)

    def output_of(query_in, key_in, value_in, rate_in, key_start, value_start):
        return mixer_heads(
            query_in, key_in, value_in, rate_in, segment, last_prev, key_start, value_start
        )

    _, pull_output = jax.vjp(output_of, query_h, key_h, value_h, rate_h, key_init, value_init)
    grad_query_h, grad_key_h, grad_value_h, grad_rate_h, key_grad_init, value_grad_init = (
        pull_output(grad_mixed_h)
    )
    continue_end = (segment[-1] == last_prev).astype(jnp.float32) * through
    key_after = zero_state
    value_after = zero_state
    for rounds in range(lax.axis_size("seq") - 1):
        key_after, value_after = shifted(
            (
                key_grad_init + continue_end[..., None] * key_after,
                value_grad_init + continue_end[..., None] * value_after,
            ),
            "seq",
            -1,
        )

    def ends_of(key_in, value_in, rate_in):
        return ends_heads(key_in, value_in, rate_in, segment, last_prev, key_init, value_init)

    _, pull_end = jax.vjp(ends_of, key_h, value_h, rate_h)
    more_key, more_value, more_rate = pull_end((key_after, value_after))
    grad_query_rows = from_heads(grad_query_h).astype(jnp.bfloat16)
    grad_key_rows = from_heads(grad_key_h + more_key).astype(jnp.bfloat16)
    grad_value_rows = from_heads(grad_value_h + more_value).astype(jnp.bfloat16)
    grad_rate = from_heads(grad_rate_h + more_rate)
    grad_logit = (grad_rate * jax.nn.sigmoid(-forget_logit) / TAU_GATE).astype(jnp.bfloat16)
    term_bias = jnp.sum(grad_logit.astype(jnp.float32), axis=0)
    term_expand = jnp.einsum("tr,tm->rm", reduced, grad_logit, preferred_element_type=jnp.float32)
    grad_reduced = jnp.einsum(
        "tm,rm->tr", grad_logit, w_expand, preferred_element_type=jnp.float32
    ).astype(jnp.bfloat16)
    term_squeeze = jnp.einsum("td,tr->dr", normed, grad_reduced, preferred_element_type=jnp.float32)
    term_query = jnp.einsum(
        "td,te->de", normed, grad_query_rows, preferred_element_type=jnp.float32
    )
    term_key = jnp.einsum("td,te->de", normed, grad_key_rows, preferred_element_type=jnp.float32)
    term_value = jnp.einsum(
        "td,te->de", normed, grad_value_rows, preferred_element_type=jnp.float32
    )
    term_swish = jnp.einsum("td,te->de", normed, grad_swishpre, preferred_element_type=jnp.float32)
    term_output = jnp.einsum("td,te->de", gated, grad_branch, preferred_element_type=jnp.float32)
    grad_normed = (
        jnp.einsum("te,de->td", grad_query_rows, w_query, preferred_element_type=jnp.float32)
        + jnp.einsum("te,de->td", grad_key_rows, w_key, preferred_element_type=jnp.float32)
        + jnp.einsum("te,de->td", grad_value_rows, w_value, preferred_element_type=jnp.float32)
        + jnp.einsum("te,de->td", grad_swishpre, w_swish, preferred_element_type=jnp.float32)
        + jnp.einsum("tr,dr->td", grad_reduced, w_squeeze, preferred_element_type=jnp.float32)
    )
    term_mixer = jnp.sum(grad_normed * inputs_f * scale_one, axis=0)
    scaled_one = grad_normed * gain_onef
    grad_inputs = (
        grad_hidden
        + scale_one * scaled_one
        - inputs_f * scale_one**3 * jnp.mean(scaled_one * inputs_f, axis=-1, keepdims=True)
    )
    mixer_grads = (
        lax.psum_scatter(term_query, ("seq", "batch"), scatter_dimension=0, tiled=True),
        lax.psum_scatter(term_key, ("seq", "batch"), scatter_dimension=0, tiled=True),
        lax.psum_scatter(term_value, ("seq", "batch"), scatter_dimension=0, tiled=True),
        lax.psum_scatter(term_swish, ("seq", "batch"), scatter_dimension=0, tiled=True),
        lax.psum_scatter(term_output, ("seq", "batch"), scatter_dimension=0, tiled=True),
        lax.psum_scatter(term_squeeze, ("seq", "batch"), scatter_dimension=0, tiled=True),
        lax.psum_scatter(term_expand, ("seq", "batch"), scatter_dimension=1, tiled=True),
        lax.psum_scatter(term_bias, ("seq", "batch"), scatter_dimension=0, tiled=True),
        lax.psum_scatter(term_mixer, ("seq", "batch"), scatter_dimension=0, tiled=True),
        lax.psum_scatter(term_head, ("seq", "batch"), scatter_dimension=0, tiled=True),
    )
    (
        query_share,
        key_share,
        value_share,
        swish_share,
        output_share,
        squeeze_share,
        expand_share,
        bias_share,
        mixer_gain_share,
        head_share,
    ) = mixer_grads
    grad_input = grad_inputs.astype(jnp.bfloat16).reshape(1, row_count, model_width)
    return (
        layer_output,
        grad_input,
        mixer_gain_share,
        query_share,
        key_share,
        value_share,
        squeeze_share,
        expand_share,
        bias_share,
        swish_share,
        head_share,
        output_share,
        feed_share,
        gate_share,
        up_share,
        down_share,
    )


def solution(mesh):
    in_specs = (
        P("batch", "seq", None),
        P("batch", "seq"),
        P(("seq", "batch")),
        P(("seq", "batch"), None),
        P(("seq", "batch"), None),
        P(("seq", "batch"), None),
        P(("seq", "batch"), None),
        P(None, ("seq", "batch")),
        P(("seq", "batch")),
        P(("seq", "batch"), None),
        P(("seq", "batch")),
        P(("seq", "batch"), None),
        P(("seq", "batch")),
        P(("seq", "batch"), None),
        P(("seq", "batch"), None),
        P(("seq", "batch"), None),
        P("batch", "seq", None),
    )
    out_specs = (
        P("batch", "seq", None),
        P("batch", "seq", None),
        P(("seq", "batch")),
        P(("seq", "batch"), None),
        P(("seq", "batch"), None),
        P(("seq", "batch"), None),
        P(("seq", "batch"), None),
        P(None, ("seq", "batch")),
        P(("seq", "batch")),
        P(("seq", "batch"), None),
        P(("seq", "batch")),
        P(("seq", "batch"), None),
        P(("seq", "batch")),
        P(("seq", "batch"), None),
        P(("seq", "batch"), None),
        P(("seq", "batch"), None),
    )
    return jax.shard_map(local, mesh=mesh, in_specs=in_specs, out_specs=out_specs, check_vma=False)
```

profile of v0, /device:TPU:0, one launch (start us, length us, event | category | flops | bytes accessed | tf_op | source)
XLA Modules:
  0.0 4052.3 jit_solution(15255022894072189090)
XLA Ops:
  19.7 40.0 all-reduce.12
  59.7 42.1 %all-gather = bf16[32,64,16]{1,2,0:T(8,128)(2,1)S(1)} all-gather(bf16[1,64,16]{1,2,0:T(8,128)(2,1)S(1)} %bitcast.982), channel_id=1, replica_groups=mesh['seq'=4,'batch'=8] {'seq','batch'}, dimensions={0}, use_global_device_ids=true | all-gather | bytes 67584 | tf_op jit(solution)/shard_map/all_gather | solution.py:128
  102.1 37.3 all_gather.57
  153.3 18.1 all-gather.12.cloned.1.call-done
  179.9 21.8 while.91
  218.3 16.4 collective-permute-done.1
  256.1 10.8 collective-permute-done.2
  287.3 17.1 collective-permute-done.6
  304.3 217.6 %while.92 = (s32[]{:T(128)}, f32[4,256,512]{2,1,0:T(8,128)S(1)}, f32[256]{0:T(256)S(1)}, f32[4,256,64]{1,2,0:T(8,128)S(1)}, f32[4,256,512]{2,1,0:T(8,128)}, /*in...) while((s32[]{:T(128)}, f32[4,256,512]{2,1,0:T(8,128)S(1)}, ...), condition=%wide.region_12.13_spmd, body=%wide.region_7.12_spmd.sunk | while | flops 1143668992 | bytes 8295481 | solution.py:78
  329.9 19.3 fusion.417
  355.5 12.6 fusion.421
  377.7 19.2 fusion.417
  403.2 12.6 fusion.421
  425.5 19.3 fusion.417
  451.0 12.6 fusion.421
  473.2 19.2 fusion.417
  498.7 12.6 fusion.421
  540.1 33.9 all-gather.20.cloned.1.call-done
  574.0 13.1 fusion.249
  587.1 132.6 %all-gather.22.cloned.1.call-done = bf16[2048,5632]{1,0:T(8,128)(2,1)} async-done(((bf16[64,5632]{1,0:T(8,128)(2,1)}), bf16[2048,5632]{1,0:T(8,128)(2,1)}) %all-gather.22.cloned.1.call-update) | async-done | bytes 23068688 | tf_op jit(solution)/shard_map/all_gather | solution.py:196
  719.7 13.3 fusion.250
  732.9 132.4 %all-gather.24.cloned.1.call-done = bf16[5632,2048]{1,0:T(8,128)(2,1)} async-done(((bf16[176,2048]{1,0:T(8,128)(2,1)}), bf16[5632,2048]{1,0:T(8,128)(2,1)}) %all-gather.24.cloned.1.call-update) | async-done | bytes 23068688 | tf_op jit(solution)/shard_map/all_gather | solution.py:197
  865.4 18.6 multiply_convert_fusion
  883.9 12.6 fusion.251
  896.5 14.6 multiply_reduce_fusion.2
  930.0 430.3 %while.93 = (s32[]{:T(128)}, bf16[4,256,512]{1,2,0:T(8,128)(2,1)}, f32[4,256,512]{1,2,0:T(8,128)}, f32[4,256,512]{1,2,0:T(8,128)}, f32[4,256,64]{1,2,0:T(8,128)}...) while((s32[]{:T(128)}, bf16[4,256,512]{1,2,0:T(8,128)(2,1)}, ...), condition=%wide.region_28.29_spmd, body=%wide.region_17.28_spmd.sunk | while | flops 2849539072 | bytes 33079996 | solution.py:78
  938.5 19.4 fusion.451
  961.6 16.5 fusion.455
  980.2 13.0 fusion.457
  998.0 12.7 fusion.461
  1013.4 15.2 fusion.463
  1044.0 19.4 fusion.451
  1067.1 16.5 fusion.455
  1085.7 13.0 fusion.457
  1103.5 12.7 fusion.461
  1118.9 15.2 fusion.463
  1149.5 19.4 fusion.451
  1172.5 16.5 fusion.455
  1191.1 13.0 fusion.457
  1208.9 12.7 fusion.461
  1224.3 15.2 fusion.463
  1254.9 19.4 fusion.451
  1277.9 16.5 fusion.455
  1296.5 13.0 fusion.457
  1314.4 12.7 fusion.461
  1329.8 15.2 fusion.463
  1364.2 14.0 collective-permute-done.10
  1389.5 10.6 collective-permute-done.11
  1405.0 12.9 collective-permute-done.8
  1429.2 9.9 collective-permute-done.9
  1441.6 53.6 %while.95 = (s32[]{:T(128)}, f32[4,256,512]{1,2,0:T(8,128)S(1)}, f32[4,256,512]{1,2,0:T(8,128)}, f32[4,256,64]{1,2,0:T(8,128)}, f32[4,64,256]{2,1,0:T(8,128)}, /...) while((s32[]{:T(128)}, f32[4,256,512]{1,2,0:T(8,128)S(1)}, ...), condition=%wide.region_39.40_spmd.clone, body=%wide.region_33.39_spmd.clone.sunk | while | flops 405094592 | bytes 4274673 | solution.py:90
  1557.1 19.7 fusion.254
  1577.2 19.7 fusion.255
  1598.2 19.9 fusion.211
  1625.2 12.5 fusion.190
  1654.9 45.9 %all-reduce.11 = (f32[2048]{0:T(1024)S(1)}, f32[16,256]{0,1:T(8,128)}, f32[256]{0:T(256)S(1)}, f32[2048]{0:T(1024)S(1)}, f32[2048]{0:T(1024)S(1)}) all-reduce(f32[2048]{0:T(1024)S(1)} %get-tuple-element.1173, f32[16,256]{0,1:T(8,128)S(1)} %fusion.253, ...), channel_id=2, replica_groups=mesh['seq'=4,'batch'=8] {'seq','batch'}, use_global_device_ids=true, to_apply=%region_42.43.clone | all-reduce | flops 10496 | bytes 83968
  1709.1 112.3 %reduce-scatter.12.cloned.1.call-done = f32[64,2048]{1,0:T(8,128)} async-done(((f32[2048,2048]{1,0:T(8,128)}), f32[64,2048]{1,0:T(8,128)}) %reduce-scatter.12.cloned.1.call-update) | async-done | bytes 524304 | tf_op jit(solution)/shard_map/reduce_scatter | solution.py:341
  1821.3 187.4 %reduce-scatter.18.cloned.1.call-done = f32[64,2048]{1,0:T(8,128)} async-done(((f32[2048,2048]{1,0:T(8,128)}), f32[64,2048]{1,0:T(8,128)}) %reduce-scatter.18.cloned.1.call-update) | async-done | bytes 524304 | tf_op jit(solution)/shard_map/reduce_scatter | solution.py:344
  2008.7 187.2 %reduce-scatter.20.cloned.1.call-done = f32[64,2048]{1,0:T(8,128)} async-done(((f32[2048,2048]{1,0:T(8,128)}), f32[64,2048]{1,0:T(8,128)}) %reduce-scatter.20.cloned.1.call-update) | async-done | bytes 524304 | tf_op jit(solution)/shard_map/reduce_scatter | solution.py:345
  2195.9 187.3 %reduce-scatter.14.cloned.1.call-done = f32[64,2048]{1,0:T(8,128)} async-done(((f32[2048,2048]{1,0:T(8,128)}), f32[64,2048]{1,0:T(8,128)}) %reduce-scatter.14.cloned.1.call-update) | async-done | bytes 524304 | tf_op jit(solution)/shard_map/reduce_scatter | solution.py:342
  2383.3 187.2 %reduce-scatter.16.cloned.1.call-done = f32[64,2048]{1,0:T(8,128)} async-done(((f32[2048,2048]{1,0:T(8,128)}), f32[64,2048]{1,0:T(8,128)}) %reduce-scatter.16.cloned.1.call-update) | async-done | bytes 524304 | tf_op jit(solution)/shard_map/reduce_scatter | solution.py:343
  2570.5 492.5 %reduce-scatter.22.cloned.1.call-done = f32[64,5632]{1,0:T(8,128)} async-done(((f32[2048,5632]{1,0:T(8,128)}), f32[64,5632]{1,0:T(8,128)}) %reduce-scatter.22.cloned.1.call-update) | async-done | bytes 1441808 | tf_op jit(solution)/shard_map/reduce_scatter | solution.py:236
  3062.9 491.3 %reduce-scatter.24.cloned.1.call-done = f32[64,5632]{1,0:T(8,128)} async-done(((f32[2048,5632]{1,0:T(8,128)}), f32[64,5632]{1,0:T(8,128)}) %reduce-scatter.24.cloned.1.call-update) | async-done | bytes 1441808 | tf_op jit(solution)/shard_map/reduce_scatter | solution.py:237
  3554.2 491.3 %reduce-scatter.26.cloned.1.call-done = f32[176,2048]{1,0:T(8,128)} async-done(((f32[5632,2048]{1,0:T(8,128)}), f32[176,2048]{1,0:T(8,128)}) %reduce-scatter.26.cloned.1.call-update) | async-done | bytes 1441808 | tf_op jit(solution)/shard_map/reduce_scatter | solution.py:238
  (865 shorter events, 515.7 us)
Async XLA Ops:
  7.2 52.5 %copy-start.77 = (bf16[64,16]{0,1:T(8,128)(2,1)S(1)}, bf16[64,16]{0,1:T(8,128)(2,1)}, u32[]{:S(2)}) copy-start(bf16[64,16]{0,1:T(8,128)(2,1)} %param.33) | copy-start | bytes 6148
  7.2 94.8 %copy-start.80 = (bf16[16,8]{0,1:T(8,128)(2,1)S(1)}, bf16[16,8]{0,1:T(8,128)(2,1)}, u32[]{:S(2)}) copy-start(bf16[16,8]{0,1:T(8,128)(2,1)} %param.34) | copy-start | bytes 772
  7.3 132.2 %copy-start = (bf16[1,256,2048]{2,1,0:T(8,128)(2,1)S(1)}, bf16[1,256,2048]{2,1,0:T(8,128)(2,1)}, u32[]{:S(2)}) copy-start(bf16[1,256,2048]{2,1,0:T(8,128)(2,1)} %param.27) | copy-start | bytes 3145732
  7.3 140.2 %all-gather.14.cloned.1.call-start = ((), (), s32[]{:S(2)}) async-start(), calls=%async_computation.11 | async-start | bytes 8650752 | tf_op jit(solution)/shard_map/all_gather | solution.py:125
  8.0 163.4 %all-gather.12.cloned.1.call-start = ((), (), s32[]{:S(2)}) async-start(), calls=%async_computation.10 | async-start | bytes 8650752 | tf_op jit(solution)/shard_map/all_gather | solution.py:124
  8.7 270.4 %all-gather.10.cloned.1.call-start = ((), (), s32[]{:S(2)}) async-start(), calls=%async_computation.9 | async-start | bytes 8650752 | tf_op jit(solution)/shard_map/all_gather | solution.py:123
  9.5 514.4 %all-gather.16.cloned.1.call-start = ((), (), s32[]{:S(2)}) async-start(), calls=%async_computation.12 | async-start | bytes 8650752 | tf_op jit(solution)/shard_map/all_gather | solution.py:126
  10.1 522.2 %all-gather.18.cloned.1.call-start = ((), (), s32[]{:S(2)}) async-start(), calls=%async_computation.13 | async-start | bytes 8650752 | tf_op jit(solution)/shard_map/all_gather | solution.py:127
  10.6 563.3 %all-gather.20.cloned.1.call-start = ((), (), s32[]{:S(2)}) async-start(), calls=%async_computation.14 | async-start | bytes 23789568 | tf_op jit(solution)/shard_map/all_gather | solution.py:195
  11.2 708.4 %all-gather.22.cloned.1.call-start = ((), (), s32[]{:S(2)}) async-start(), calls=%async_computation.15 | async-start | bytes 23789568 | tf_op jit(solution)/shard_map/all_gather | solution.py:196
  12.0 853.4 %all-gather.24.cloned.1.call-start = ((), (), s32[]{:S(2)}) async-start(), calls=%async_computation.16 | async-start | bytes 23789568 | tf_op jit(solution)/shard_map/all_gather | solution.py:197
  12.7 1694.9 %reduce-scatter.28.cloned.1.call-start = ((), (), s32[]{:S(2)}) async-start(), calls=%async_computation.25 | async-start | bytes 1081344
  13.4 132.6 %collective-permute-start = (f32[1]{0:T(128)}, f32[1]{0:T(128)}, u32[]{:S(2)}, u32[]{:S(2)}) collective-permute-start(f32[1]{0:T(128)} %bitcast.59), channel_id=1, source_target_pairs={{0,8},{8,16},{16,24},{1,9},{9,17},{17,25},{2,10},{10,18},{18,26},{... | collective-permute-start | bytes 20 | tf_op jit(solution)/shard_map/ppermute | solution.py:17
  102.0 38.3 copy-start.53
  102.1 421.8 %copy-start.48 = (f32[2048]{0:T(1024)}, f32[2048]{0:T(1024)S(1)}, u32[]{:S(2)}) copy-start(f32[2048]{0:T(1024)S(1)} %convert_element_type.214) | copy-start | bytes 24580
  140.3 138.9 %copy-start.61 = (f32[256]{0:T(256)}, f32[256]{0:T(256)S(1)}, u32[]{:S(2)}) copy-start(f32[256]{0:T(256)S(1)} %get-tuple-element.1369) | copy-start | bytes 3076
  147.5 119.3 %copy-start.65 = (f32[4,64]{1,0:T(4,128)}, f32[4,64]{1,0:T(4,128)S(1)}, u32[]{:S(2)}) copy-start(f32[4,64]{1,0:T(4,128)S(1)} %get-tuple-element.1175) | copy-start | bytes 3076
  201.8 34.1 copy-start.13
  201.8 34.1 copy-start.14
  201.9 16.4 collective-permute-start.4
  205.2 29.5 collective-permute-start.1
  235.9 20.2 collective-permute-start.5
  241.1 25.7 collective-permute-start.2
  269.5 17.8 collective-permute-start.3
  274.7 29.7 collective-permute-start.6
  327.3 21.9 copy-start.51
  327.4 21.8 copy-start.23
  375.0 22.0 copy-start.51
  375.1 21.9 copy-start.23
  422.8 22.0 copy-start.51
  422.9 21.9 copy-start.23
  470.5 21.9 copy-start.51
  470.6 21.8 copy-start.23
  540.0 179.6 %copy-start.5 = (bf16[256,2048]{1,0:T(8,128)(2,1)}, bf16[256,2048]{1,0:T(8,128)(2,1)S(1)}, u32[]{:S(2)}) copy-start(bf16[256,2048]{1,0:T(8,128)(2,1)S(1)} %multiply_convert_fusion.4) | copy-start | bytes 3145732
  934.7 23.3 copy-start.38
  935.5 22.4 copy-start.36
  1040.2 23.3 copy-start.38
  1041.0 22.4 copy-start.36
  1145.6 23.3 copy-start.38
  1146.4 22.4 copy-start.36
  1251.0 23.3 copy-start.38
  1251.9 22.4 copy-start.36
  1361.6 16.6 collective-permute-start.10
  1362.9 40.1 copy-start.79
  1362.9 26.6 collective-permute-start.7
  1378.4 21.7 collective-permute-start.11
  1401.1 16.8 collective-permute-start.8
  1403.7 25.5 collective-permute-start.12
  1418.8 20.3 collective-permute-start.9
  1441.6 56.7 %copy-start.56 = (bf16[16,256]{0,1:T(8,128)(2,1)S(1)}, bf16[16,256]{0,1:T(8,128)(2,1)}, u32[]{:S(2)}) copy-start(bf16[16,256]{0,1:T(8,128)(2,1)} %copy-done.55) | copy-start | bytes 24580
  1441.6 56.9 %copy-start.1 = (bf16[1,256,2048]{2,1,0:T(8,128)(2,1)S(1)}, bf16[1,256,2048]{2,1,0:T(8,128)(2,1)}, u32[]{:S(2)}) copy-start(bf16[1,256,2048]{2,1,0:T(8,128)(2,1)} %param.27) | copy-start | bytes 3145732
  1441.6 56.9 %copy-start.49 = (f32[2048]{0:T(1024)S(1)}, f32[2048]{0:T(1024)}, u32[]{:S(2)}) copy-start(f32[2048]{0:T(1024)} %copy-done.48) | copy-start | bytes 24580
  1441.6 56.9 %copy-start.63 = (f32[256]{0:T(256)S(1)}, f32[256]{0:T(256)}, u32[]{:S(2)}) copy-start(f32[256]{0:T(256)} %copy-done.61) | copy-start | bytes 3076
  1500.2 321.1 %reduce-scatter.12.cloned.1.call-start = ((), (), s32[]{:S(2)}) async-start(), calls=%async_computation.17 | async-start | bytes 17301504 | tf_op jit(solution)/shard_map/reduce_scatter | solution.py:341
  1509.8 498.9 %reduce-scatter.18.cloned.1.call-start = ((), (), s32[]{:S(2)}) async-start(), calls=%async_computation.20 | async-start | bytes 17301504 | tf_op jit(solution)/shard_map/reduce_scatter | solution.py:344
  1519.3 676.6 %reduce-scatter.20.cloned.1.call-start = ((), (), s32[]{:S(2)}) async-start(), calls=%async_computation.21 | async-start | bytes 17301504 | tf_op jit(solution)/shard_map/reduce_scatter | solution.py:345
  1530.4 852.9 %reduce-scatter.14.cloned.1.call-start = ((), (), s32[]{:S(2)}) async-start(), calls=%async_computation.18 | async-start | bytes 17301504 | tf_op jit(solution)/shard_map/reduce_scatter | solution.py:342
  1543.1 1027.3 %reduce-scatter.16.cloned.1.call-start = ((), (), s32[]{:S(2)}) async-start(), calls=%async_computation.19 | async-start | bytes 17301504 | tf_op jit(solution)/shard_map/reduce_scatter | solution.py:343
  1555.9 1507.0 %reduce-scatter.22.cloned.1.call-start = ((), (), s32[]{:S(2)}) async-start(), calls=%async_computation.22 | async-start | bytes 47579136 | tf_op jit(solution)/shard_map/reduce_scatter | solution.py:236
  1576.8 1977.4 %reduce-scatter.24.cloned.1.call-start = ((), (), s32[]{:S(2)}) async-start(), calls=%async_computation.23 | async-start | bytes 47579136 | tf_op jit(solution)/shard_map/reduce_scatter | solution.py:237
  1597.0 2448.6 %reduce-scatter.26.cloned.1.call-start = ((), (), s32[]{:S(2)}) async-start(), calls=%async_computation.24 | async-start | bytes 47579136 | tf_op jit(solution)/shard_map/reduce_scatter | solution.py:238
  1619.3 25.0 slice-start
  1652.8 51.7 %copy-start.4 = (f32[256,2048]{1,0:T(8,128)S(1)}, f32[256,2048]{1,0:T(8,128)}, u32[]{:S(2)}) copy-start(f32[256,2048]{1,0:T(8,128)} %copy-done.2) | copy-start | bytes 6291460
  1652.8 51.6 %copy-start.76 = (f32[256]{0:T(256)S(1)}, f32[256]{0:T(256)}, u32[]{:S(2)}) copy-start(f32[256]{0:T(256)} %get-tuple-element.1368) | copy-start | bytes 3076
  (120 other events, 836.6 us)
Sparse Core Ops, SparseCore 0:
  11.1 80.4 all-gather.13
  94.6 76.7 all-gather.11
  174.4 87.9 all-gather.9
  265.3 83.7 all-gather.15
  351.9 76.0 all-gather.17
  430.7 143.2 all-gather.19
  576.8 142.7 all-gather.21
  722.5 142.7 all-gather.23
  1500.3 134.2 reduce-scatter.27
  1637.4 183.9 reduce-scatter.11
  1824.3 184.3 reduce-scatter.17
  2011.5 184.3 reduce-scatter.19
  2198.9 184.3 reduce-scatter.13
  2386.1 184.3 reduce-scatter.15
  2573.3 489.5 reduce-scatter.21
  3065.8 488.4 reduce-scatter.23
  3557.0 488.4 reduce-scatter.25
where the time goes:
time: 4070 us; the launch traced here: 4050 us
  waiting for transfers between devices  2780 us (68%)
  matrix products  737 us (18%)
  other arithmetic  177 us (4%)
  blocking collectives  165 us (4%)
  local copies, waits for them, and re-layouts  98.2 us (2%)
    reduce_scatter x1, waiting for transfers between devices, local(): lax.psum_scatter(term_gate, ('seq', 'batch'), scatter_dimension=0, tiled=...  492 us
    reduce_scatter x1, waiting for transfers between devices, local(): lax.psum_scatter(term_down, ('seq', 'batch'), scatter_dimension=0, tiled=...  491 us
    reduce_scatter x1, waiting for transfers between devices, local(): lax.psum_scatter(term_up, ('seq', 'batch'), scatter_dimension=0, tiled=True)  491 us
    dot_general x12, matrix products, head_output(): jnp.einsum('tsm,ts->tm', weight, scores, precision=lax.Precision.HIGHEST)  207 us
    reduce_scatter x1, waiting for transfers between devices, local(): lax.psum_scatter(term_swish, ('seq', 'batch'), scatter_dimension=0, tiled...  187 us
    reduce_scatter x1, waiting for transfers between devices, local(): lax.psum_scatter(term_key, ('seq', 'batch'), scatter_dimension=0, tiled=T...  187 us
    reduce_scatter x1, waiting for transfers between devices, local(): lax.psum_scatter(term_output, ('seq', 'batch'), scatter_dimension=0, tile...  187 us
    reduce_scatter x1, waiting for transfers between devices, local(): lax.psum_scatter(term_value, ('seq', 'batch'), scatter_dimension=0, tiled...  187 us
  transfers between devices with their start and end apart: 30, of which 23 were waited for; matrix products, arithmetic and copies ran while one was open for 11% of the time, Pallas kernels for 0%

commit v1 on v0

v1 whole, which is shorter than its diff:
```python
import functools

import jax
import jax.numpy as jnp
import numpy as np
from jax import lax
from jax.experimental import pallas as pl
from jax.experimental.pallas import tpu as pltpu
from jax.sharding import PartitionSpec as P

HEADS = 4
SLOTS = 64
RANK = 16
EPS = 1e-06
TAU_GATE = 8.0
CHUNK = 128
SUB = 16
BOTH = ("seq", "batch")
F32 = jnp.float32
BF16 = jnp.bfloat16
HIGHEST = lax.Precision.HIGHEST


def dot_nn(left, right):
    return lax.dot_general(left, right, (((1,), (0,)), ((), ())), preferred_element_type=F32)


def dot_nt(left, right):
    return lax.dot_general(left, right, (((1,), (1,)), ((), ())), preferred_element_type=F32)


def dot_tn(left, right):
    return lax.dot_general(left, right, (((0,), (0,)), ((), ())), preferred_element_type=F32)


def exact_nn(left, right):
    return lax.dot_general(
        left, right, (((1,), (0,)), ((), ())), precision=HIGHEST, preferred_element_type=F32
    )


def exact_nt(left, right):
    return lax.dot_general(
        left, right, (((1,), (1,)), ((), ())), precision=HIGHEST, preferred_element_type=F32
    )


def halves(value):
    high = value.astype(BF16)
    return high, (value - high.astype(F32)).astype(BF16)


def split_nn(left, right):
    high, rest = halves(left)
    return dot_nn(high, right) + dot_nn(rest, right)


def split_nt(left, right):
    high, rest = halves(left)
    return dot_nt(high, right) + dot_nt(rest, right)


def chunk_tables():
    at = np.arange(CHUNK)
    sums, covers = [], []
    half = SUB
    while half < CHUNK:
        right = (at // half) % 2 == 1
        edge = (at // (2 * half)) * 2 * half + half - 1
        low = np.where(right, edge, at)
        high = np.where(right, at, edge)
        sums.append((at[:, None] > low[None, :]) & (at[:, None] <= high[None, :]))
        same = (at[:, None] // (2 * half)) == (at[None, :] // (2 * half))
        covers.append(same & ~right[:, None] & right[None, :])
        half *= 2
    sums.append(at[:, None] <= at[None, :])
    sums.append(at[:, None] > at[None, :])
    apart = at[None, :] - at[:, None]
    apart = np.where(at[None, :] // SUB == at[:, None] // SUB, apart, -1)
    return (
        np.concatenate(sums, axis=1).astype(np.float32),
        np.stack(covers).astype(np.float32),
        np.maximum(apart, -1).astype(np.int32),
    )


def rolled(value, by):
    return value if by % CHUNK == 0 else pltpu.roll(value, by % CHUNK, 1)


def exponents(rate, sums):
    return jnp.exp(exact_nn(rate, sums))


def piece(value, at):
    return value[:, at * CHUNK : (at + 1) * CHUNK]


def mixer_forward_kernel(
    levels,
    factor,
    mine,
    query,
    key,
    value,
    rate,
    inflow,
    rows,
    segment_col,
    sums,
    covers,
    apart,
    output,
    attention_out,
    logits_out,
    key_start,
    value_start,
    key_state,
    value_state,
):
    @pl.when(pl.program_id(0) == 0)
    def _():
        key_state[...] = jnp.zeros_like(key_state)
        value_state[...] = jnp.zeros_like(value_state)

    key_in, value_in = key_state[...], value_state[...]
    key_start[0] = key_in
    value_start[0] = value_in
    q, k, v = query[...], key[...], value[...]
    a, g = rate[...], inflow[...]
    decay = exponents(a, sums[...])
    before, after = piece(decay, levels), piece(decay, levels + 1)
    carried = before * rows[1:2, :]
    visible = segment_col[...] == rows[0:1, :]
    scores = jnp.where(visible, dot_nt(k, q) * factor, 0.0)
    logits = carried * (split_nt(key_in, q) * factor)
    for level in range(levels):
        part = piece(decay, level)
        logits = logits + part * exact_nn(part * g, scores * covers[level])
    gap = apart[...]
    total = jnp.zeros_like(a)
    weights = []
    for by in range(SUB):
        if by:
            total = total + rolled(a, by - 1)
        weight = jnp.exp(total) * rolled(g, by)
        weights.append(weight)
        logits = logits + weight * jnp.sum(
            jnp.where(gap == by, scores, 0.0), axis=0, keepdims=True
        )
    attention = jnp.exp(logits - jnp.max(logits, axis=0, keepdims=True))
    attention = attention / jnp.sum(attention, axis=0, keepdims=True)
    attention_out[...] = attention
    logits_out[...] = logits
    mixing = jnp.zeros((CHUNK, CHUNK), F32)
    for level in range(levels):
        part = piece(decay, level)
        mixing = mixing + covers[level] * dot_tn(
            (part * g).astype(BF16), (part * attention).astype(BF16)
        )
    for by in range(SUB):
        row = jnp.sum(weights[by] * attention, axis=0, keepdims=True)
        mixing = jnp.where(gap == by, row, mixing)
    mixing = jnp.where(visible, mixing, 0.0).astype(BF16)
    output[...] = dot_tn(mixing, v) + dot_tn(
        (carried * attention).astype(BF16), value_in.astype(BF16)
    )
    ends = after * g * rows[2:3, :]
    keep = carried[:, CHUNK - 1 : CHUNK]
    key_state[...] = keep * key_in + split_nn(ends, k)
    value_state[...] = keep * value_in + split_nn(ends, v)


def mixer_backward_kernel(
    levels,
    factor,
    mine,
    query,
    key,
    value,
    grad_output,
    rate,
    inflow,
    rows,
    segment_col,
    sums,
    covers,
    apart,
    later,
    attention_in,
    logits_in,
    key_start,
    value_start,
    grad_query,
    grad_key,
    grad_value,
    grad_rate,
    key_grad,
    value_grad,
    flow,
):
    @pl.when(pl.program_id(0) == 0)
    def _():
        key_grad[...] = jnp.zeros_like(key_grad)
        value_grad[...] = jnp.zeros_like(value_grad)
        flow[...] = jnp.zeros_like(flow)

    key_in, value_in = key_start[0], value_start[0]
    key_after, value_after = key_grad[...], value_grad[...]
    q, k, v, d = query[...], key[...], value[...], grad_output[...]
    a, g = rate[...], inflow[...]
    attention, logits = attention_in[...], logits_in[...]
    decay = exponents(a, sums[...])
    before, after = piece(decay, levels), piece(decay, levels + 1)
    carried = before * rows[1:2, :]
    visible = segment_col[...] == rows[0:1, :]
    scores = jnp.where(visible, dot_nt(k, q) * factor, 0.0)
    reads = jnp.where(visible, dot_nt(v, d), 0.0)
    gap = apart[...]
    grad_att = carried * split_nt(value_in, d)
    for level in range(levels):
        part = piece(decay, level)
        grad_att = grad_att + part * exact_nn(part * g, reads * covers[level])
    total = jnp.zeros_like(a)
    bare, weights, score_rows, read_rows = [], [], [], []
    for by in range(SUB):
        if by:
            total = total + rolled(a, by - 1)
        bare.append(jnp.exp(total))
        weights.append(bare[by] * rolled(g, by))
        score_rows.append(jnp.sum(jnp.where(gap == by, scores, 0.0), axis=0, keepdims=True))
        read_rows.append(jnp.sum(jnp.where(gap == by, reads, 0.0), axis=0, keepdims=True))
        grad_att = grad_att + weights[by] * read_rows[by]
    grad_logits = attention * (
        grad_att - jnp.sum(attention * grad_att, axis=0, keepdims=True)
    )
    mixing = jnp.zeros((CHUNK, CHUNK), F32)
    spread = jnp.zeros((CHUNK, CHUNK), F32)
    ends = after * rows[2:3, :]
    grad_inflow = ends * (split_nt(key_after, k) + split_nt(value_after, v))
    for level in range(levels):
        part = piece(decay, level)
        left = (part * g).astype(BF16)
        att_part, log_part = part * attention, part * grad_logits
        mixing = mixing + covers[level] * dot_tn(left, att_part.astype(BF16))
        spread = spread + covers[level] * dot_tn(left, log_part.astype(BF16))
        grad_inflow = grad_inflow + part * (
            exact_nt(log_part, scores * covers[level]) + exact_nt(att_part, reads * covers[level])
        )
    for by in range(SUB):
        row = jnp.sum(weights[by] * attention, axis=0, keepdims=True)
        mixing = jnp.where(gap == by, row, mixing)
        row = jnp.sum(weights[by] * grad_logits, axis=0, keepdims=True)
        spread = jnp.where(gap == by, row, spread)
        terms = bare[by] * (grad_logits * score_rows[by] + attention * read_rows[by])
        grad_inflow = grad_inflow + rolled(terms, -by)
    mixing = jnp.where(visible, mixing, 0.0).astype(BF16)
    spread = (jnp.where(visible, spread, 0.0) * factor).astype(BF16)
    log_carried = carried * grad_logits * factor
    att_carried = carried * attention
    ends = (ends * g).astype(BF16)
    grad_query[...] = (
        dot_tn(spread, k) + dot_tn(log_carried.astype(BF16), key_in.astype(BF16))
    ).astype(BF16)
    grad_key[...] = (dot_nn(spread, q) + dot_tn(ends, key_after.astype(BF16))).astype(BF16)
    grad_value[...] = (dot_nn(mixing, d) + dot_tn(ends, value_after.astype(BF16))).astype(BF16)
    change = grad_logits * logits + attention * grad_att - g * grad_inflow
    same = jnp.where(visible, later[...], 0.0)
    flows = exact_nn(change, same) + rows[2:3, :] * flow[:, 0:1]
    grad_rate[...] = rows[3:4, :] * flows - jnp.exp(a) * grad_inflow
    keep = carried[:, CHUNK - 1 : CHUNK]
    key_before = keep * key_after + split_nn(log_carried, q)
    value_before = keep * value_after + split_nn(att_carried, d)
    key_grad[...] = key_before
    value_grad[...] = value_before
    flow[...] = jnp.broadcast_to(
        jnp.sum(key_before * key_in + value_before * value_in, axis=1, keepdims=True), flow.shape
    )


def mixer_specs(length, size, ring, backward):
    count = length // CHUNK
    per = count // ring

    def natural(step):
        return count - 1 - step if backward else step

    def moved(step, mine):
        at = natural(step)
        return lax.bitwise_xor(at // per, mine[0]) * per + at % per

    wide = pl.BlockSpec((CHUNK, size), lambda step, mine: (moved(step, mine), 0))
    slim = pl.BlockSpec((SLOTS, CHUNK), lambda step, mine: (0, moved(step, mine)))
    plain = pl.BlockSpec((SLOTS, CHUNK), lambda step, mine: (0, natural(step)))
    rows = pl.BlockSpec((8, CHUNK), lambda step, mine: (0, natural(step)))
    column = pl.BlockSpec((CHUNK, 1), lambda step, mine: (natural(step), 0))
    state = pl.BlockSpec((1, SLOTS, size), lambda step, mine: (natural(step), 0, 0))
    return count, wide, slim, plain, rows, column, state


def whole(array):
    rank = array.ndim
    return pl.BlockSpec(array.shape, lambda step, mine: (0,) * rank)


def mixer_forward(mine, ring, query, key, value, rate, inflow, rows, column):
    length, size = query.shape
    sums, covers, apart = (jnp.asarray(table) for table in chunk_tables())
    count, wide, slim, plain, row_spec, col_spec, state = mixer_specs(length, size, ring, False)
    kernel = functools.partial(mixer_forward_kernel, covers.shape[0], size ** (-0.25))
    return pl.pallas_call(
        kernel,
        out_shape=(
            jax.ShapeDtypeStruct((length, size), F32),
            jax.ShapeDtypeStruct((SLOTS, length), F32),
            jax.ShapeDtypeStruct((SLOTS, length), F32),
            jax.ShapeDtypeStruct((count, SLOTS, size), F32),
            jax.ShapeDtypeStruct((count, SLOTS, size), F32),
        ),
        grid_spec=pltpu.PrefetchScalarGridSpec(
            num_scalar_prefetch=1,
            grid=(count,),
            in_specs=[
                wide, wide, wide, slim, slim, row_spec, col_spec,
                whole(sums), whole(covers), whole(apart),
            ],
            out_specs=[wide, plain, plain, state, state],
            scratch_shapes=[pltpu.VMEM((SLOTS, size), F32)] * 2,
        ),
        compiler_params=pltpu.CompilerParams(vmem_limit_bytes=32 << 20),
        cost_estimate=pl.CostEstimate(
            flops=length * size * 2000, bytes_accessed=length * size * 12, transcendentals=length * 4096
        ),
        name="mixer_forward",
    )(mine, query, key, value, rate, inflow, rows, column, sums, covers, apart)


def mixer_backward(
    mine, ring, query, key, value, grad, rate, inflow, rows, column, attention, logits, starts
):
    length, size = query.shape
    sums, covers, apart = (jnp.asarray(table) for table in chunk_tables())
    later = jnp.asarray(np.tril(np.ones((CHUNK, CHUNK), np.float32)))
    count, wide, slim, plain, row_spec, col_spec, state = mixer_specs(length, size, ring, True)
    kernel = functools.partial(mixer_backward_kernel, covers.shape[0], size ** (-0.25))
    return pl.pallas_call(
        kernel,
        out_shape=(
            jax.ShapeDtypeStruct((length, size), BF16),
            jax.ShapeDtypeStruct((length, size), BF16),
            jax.ShapeDtypeStruct((length, size), BF16),
            jax.ShapeDtypeStruct((SLOTS, length), F32),
        ),
        grid_spec=pltpu.PrefetchScalarGridSpec(
            num_scalar_prefetch=1,
            grid=(count,),
            in_specs=[
                wide, wide, wide, wide, slim, slim, row_spec, col_spec,
                whole(sums), whole(covers), whole(apart), whole(later),
                plain, plain, state, state,
            ],
            out_specs=[wide, wide, wide, slim],
            scratch_shapes=[pltpu.VMEM((SLOTS, size), F32)] * 2 + [pltpu.VMEM((SLOTS, 128), F32)],
        ),
        compiler_params=pltpu.CompilerParams(vmem_limit_bytes=32 << 20),
        cost_estimate=pl.CostEstimate(
            flops=length * size * 4000, bytes_accessed=length * size * 20, transcendentals=length * 4096
        ),
        name="mixer_backward",
    )(
        mine, query, key, value, grad, rate, inflow, rows, column,
        sums, covers, apart, later, attention, logits, *starts,
    )


def rms_scale(features):
    return lax.rsqrt(jnp.mean(features * features, axis=-1, keepdims=True) + EPS)


def swapped(block, by, ring):
    return lax.ppermute(block, "seq", [(i, i ^ by) for i in range(ring)])


def gathered(block, ring):
    return jnp.concatenate([block] + [swapped(block, by, ring) for by in range(1, ring)], axis=0)


def scattered(terms, ring):
    rows = terms.shape[0] // ring
    total = terms[:rows].astype(F32)
    for by in range(1, ring):
        total = total + swapped(terms[by * rows : (by + 1) * rows].astype(BF16), by, ring).astype(F32)
    return total


def exchanged(blocks, mine, ring):
    parts = [
        swapped(lax.dynamic_index_in_dim(blocks, mine ^ by, 0, keepdims=False), by, ring)
        if by
        else lax.dynamic_index_in_dim(blocks, mine, 0, keepdims=False)
        for by in range(ring)
    ]
    made = jnp.stack(parts)
    return jnp.concatenate(
        [lax.dynamic_index_in_dim(made, mine ^ j, 0, keepdims=True) for j in range(ring)], axis=0
    )


def local(
    layer_input,
    segments,
    mixer_gain,
    query_weight,
    key_weight,
    value_weight,
    squeeze,
    expand,
    forget_bias,
    swish_weight,
    head_gain,
    output_weight,
    feed_gain,
    gate_weight,
    up_weight,
    down_weight,
    cotangent,
):
    ring, lines = lax.axis_size("seq"), lax.axis_size("batch")
    devices = ring * lines
    mine = lax.axis_index("seq")
    rows, width = layer_input.shape[1], layer_input.shape[2]
    length = rows * ring
    own = width // devices
    head_size = width // HEADS
    copies = ring // HEADS
    part = width // ring
    head = mine // copies
    hidden_part = gate_weight.shape[1] // ring
    slots_all = HEADS * SLOTS

    def permuted(array):
        shape = array.shape[:-1]
        array = array.reshape(shape + (ring, lines, own))
        return jnp.swapaxes(array, -3, -2).reshape(shape + (width,))

    def restored(array):
        shape = array.shape[:-1]
        array = array.reshape(shape + (lines, ring, own))
        return jnp.swapaxes(array, -3, -2).reshape(shape + (width,))

    def to_order(array):
        if copies == 1:
            return array
        blocks = array.reshape((ring, rows) + array.shape[1:])
        moved = [lax.dynamic_index_in_dim(blocks, mine ^ by, 0, keepdims=False) for by in range(ring)]
        return jnp.concatenate(moved, axis=0)

    def whole_head(array):
        if copies == 1:
            return array
        full = lax.all_gather(to_order(array), "seq", axis=1, tiled=True)
        return to_order(lax.dynamic_slice_in_dim(full, head * head_size, head_size, 1))

    def own_part(array):
        if copies == 1:
            return array
        return lax.dynamic_slice_in_dim(array, (mine % copies) * part, part, 1)

    small = jnp.concatenate(
        [
            mixer_gain,
            head_gain,
            feed_gain,
            forget_bias,
            expand.T.reshape(-1),
            squeeze.reshape(-1),
        ]
    )
    small = lax.all_gather(small, BOTH, axis=0, tiled=False)
    cuts = np.cumsum([own, own, own, slots_all // devices, RANK * slots_all // devices])
    gain_one, gain_head, gain_two, bias_full, expand_t, w_squeeze = jnp.split(small, cuts, axis=1)
    gain_one = permuted(gain_one.reshape(width)).astype(F32)
    gain_head = lax.dynamic_slice_in_dim(gain_head.reshape(width), head * head_size, head_size, 0)
    gain_head = gain_head.astype(F32)
    gain_two = gain_two.reshape(width).astype(F32)
    bias_head = lax.dynamic_slice_in_dim(bias_full.reshape(slots_all), head * SLOTS, SLOTS, 0)
    expand_head = lax.dynamic_slice_in_dim(
        expand_t.reshape(slots_all, RANK), head * SLOTS, SLOTS, 0
    )
    w_squeeze = permuted(w_squeeze.reshape(width, RANK).T)

    def columns(*arrays):
        blocks = [a.reshape(own, ring, a.shape[1] // ring) for a in arrays]
        return jnp.concatenate(blocks, axis=2).transpose(1, 0, 2)

    mixer_columns = exchanged(
        columns(query_weight, key_weight, value_weight, swish_weight), mine, ring
    )
    w_mixer = lax.all_gather(mixer_columns, "batch", axis=0, tiled=False).reshape(width, 4 * part)
    w_output = lax.all_gather(output_weight, "batch", axis=0, tiled=True)
    feed_columns = exchanged(columns(gate_weight, up_weight), mine, ring)
    w_feed = lax.all_gather(feed_columns, "batch", axis=0, tiled=False).reshape(
        width, 2 * hidden_part
    )
    w_down = lax.all_gather(down_weight, "batch", axis=0, tiled=True)

    segment = lax.all_gather(segments.reshape(rows), "seq", axis=0, tiled=True).astype(F32)
    chunked = segment.reshape(-1, CHUNK)
    before = jnp.concatenate([jnp.full((1,), -1.0, F32), chunked[:-1, -1]])
    previous = jnp.concatenate([jnp.full((1,), -1.0, F32), segment[:-1]])
    mask_rows = jnp.stack(
        [
            segment,
            (chunked == before[:, None]).astype(F32).reshape(-1),
            (chunked == chunked[:, -1:]).astype(F32).reshape(-1),
            (segment == previous).astype(F32),
        ]
        + [jnp.zeros_like(segment)] * 4
    )
    segment_col = segment[:, None]

    input_own = layer_input.reshape(rows, width)
    inputs = gathered(permuted(input_own), ring).astype(F32)
    scale_one = rms_scale(inputs)
    plain_one = inputs * scale_one
    normed = (plain_one * gain_one).astype(BF16)
    mixer_pre = dot_nn(normed, w_mixer)
    query = whole_head(mixer_pre[:, :part].astype(BF16))
    key = whole_head(mixer_pre[:, part : 2 * part].astype(BF16))
    value = whole_head(mixer_pre[:, 2 * part : 3 * part].astype(BF16))
    swish_pre = whole_head(mixer_pre[:, 3 * part :])
    reduced = dot_nt(normed, w_squeeze).astype(BF16)
    forget_logit = dot_nt(expand_head, reduced) + bias_head.astype(F32)[:, None]
    log_rate = jax.nn.log_sigmoid(forget_logit) / TAU_GATE
    inflow = -jnp.expm1(log_rate)
    order = mine.reshape(1).astype(jnp.int32)
    mixed, attention, logits, key_start, value_start = mixer_forward(
        order, ring, query, key, value, log_rate, inflow, mask_rows, segment_col
    )
    head_factor = rms_scale(mixed)
    head_plain = mixed * head_factor
    head_normed = head_plain * gain_head
    swish_sig = jax.nn.sigmoid(swish_pre)
    swish_act = swish_pre * swish_sig
    gated = own_part((head_normed * swish_act).astype(BF16))
    hidden = input_own.astype(F32) + scattered(dot_nn(gated, w_output), ring)

    scale_two = rms_scale(hidden)
    feed_in = gathered(permuted((hidden * scale_two * gain_two).astype(BF16)), ring)
    feed_pre = dot_nn(feed_in, w_feed)
    gate_pre, up_pre = feed_pre[:, :hidden_part], feed_pre[:, hidden_part:]
    gate_sig = jax.nn.sigmoid(gate_pre)
    gate_act = gate_pre * gate_sig
    inner = (gate_act * up_pre).astype(BF16)
    result = hidden + scattered(dot_nn(inner, w_down), ring)
    layer_output = result.astype(BF16).reshape(1, rows, width)

    grad_own = cotangent.reshape(rows, width)
    grad_out = gathered(grad_own, ring)
    grad_inner = dot_nt(grad_out, w_down)
    grad_gatepre = grad_inner * up_pre * (gate_sig * (1.0 + gate_pre * (1.0 - gate_sig)))
    grad_feedpre = jnp.concatenate(
        [grad_gatepre.astype(BF16), (grad_inner * gate_act).astype(BF16)], axis=1
    )
    grad_feedin = restored(scattered(dot_nt(grad_feedpre, w_feed), ring))
    term_down = dot_tn(inner, grad_out).astype(BF16)
    term_feedpre = dot_tn(feed_in, grad_feedpre).astype(BF16)
    down_share = lax.psum_scatter(term_down, "batch", scatter_dimension=0, tiled=True)
    feed_share = lax.psum_scatter(term_feedpre, "batch", scatter_dimension=0, tiled=True)
    feed_share = exchanged(feed_share.reshape(ring, own, 2 * hidden_part), mine, ring)
    gate_share = feed_share[:, :, :hidden_part].transpose(1, 0, 2).reshape(own, -1)
    up_share = feed_share[:, :, hidden_part:].transpose(1, 0, 2).reshape(own, -1)
    term_feed = jnp.sum(grad_feedin * hidden * scale_two, axis=0)
    scaled_two = grad_feedin * gain_two
    grad_hidden = (
        grad_own.astype(F32)
        + scale_two * scaled_two
        - hidden * scale_two**3 * jnp.mean(scaled_two * hidden, axis=-1, keepdims=True)
    )

    grad_branch = gathered(grad_hidden.astype(BF16), ring)
    grad_gated = whole_head(dot_nt(grad_branch, w_output))
    term_output = dot_tn(gated, grad_branch).astype(BF16)
    output_share = lax.psum_scatter(term_output, "batch", scatter_dimension=0, tiled=True)
    slope = swish_sig * (1.0 + swish_pre * (1.0 - swish_sig))
    grad_swishpre = own_part((grad_gated * head_normed * slope).astype(BF16))
    grad_normed_head = grad_gated * swish_act
    term_head = jnp.sum(grad_normed_head * head_plain, axis=0) / copies
    scaled_head = grad_normed_head * gain_head
    grad_mixed = head_factor * scaled_head - mixed * head_factor**3 * jnp.mean(
        scaled_head * mixed, axis=-1, keepdims=True
    )
    grad_query, grad_key, grad_value, grad_rate = mixer_backward(
        order,
        ring,
        query,
        key,
        value,
        grad_mixed.astype(BF16),
        log_rate,
        inflow,
        mask_rows,
        segment_col,
        attention,
        logits,
        (key_start, value_start),
    )
    grad_logit = (grad_rate * jax.nn.sigmoid(-forget_logit) / TAU_GATE).astype(BF16)
    term_bias = jnp.sum(grad_logit.astype(F32), axis=1) / copies
    term_expand = dot_nn(grad_logit, reduced) / copies
    grad_reduced = (dot_tn(grad_logit, expand_head) / copies).astype(BF16)
    grad_pre = jnp.concatenate(
        [own_part(grad_query), own_part(grad_key), own_part(grad_value), grad_swishpre], axis=1
    )
    grad_normed = dot_nt(grad_pre, w_mixer) + dot_nn(grad_reduced, w_squeeze)
    term_mixer = restored(jnp.sum(grad_normed * plain_one, axis=0))
    term_squeeze = restored(dot_tn(grad_reduced, normed))
    grad_normed = restored(scattered(grad_normed, ring))
    term_pre = dot_tn(normed, grad_pre).astype(BF16)
    pre_share = lax.psum_scatter(term_pre, "batch", scatter_dimension=0, tiled=True)
    pre_share = exchanged(pre_share.reshape(ring, own, 4 * part), mine, ring)
    pre_share = pre_share.reshape(ring, own, 4, part).transpose(2, 1, 0, 3).reshape(4, own, width)
    pre_share = pre_share.astype(F32)
    inputs_own = input_own.astype(F32)
    scale_own = rms_scale(inputs_own)
    scaled_one = grad_normed * restored(gain_one)
    grad_inputs = (
        grad_hidden
        + scale_own * scaled_one
        - inputs_own * scale_own**3 * jnp.mean(scaled_one * inputs_own, axis=-1, keepdims=True)
    )
    grad_input = grad_inputs.astype(BF16).reshape(1, rows, width)

    def placed(array, size):
        full = jnp.zeros((HEADS, size) + array.shape[1:], F32)
        return lax.dynamic_update_slice_in_dim(full, array[None], head, 0)

    terms = jnp.concatenate(
        [
            term_mixer.reshape(devices, -1),
            placed(term_head, head_size).reshape(devices, -1),
            term_feed.reshape(devices, -1),
            placed(term_bias, SLOTS).reshape(devices, -1),
            placed(term_expand, SLOTS).reshape(devices, -1),
            term_squeeze.T.reshape(devices, -1),
        ],
        axis=1,
    )
    share = lax.psum_scatter(terms, BOTH, scatter_dimension=0, tiled=True)[0]
    mixer_share, head_share, feedgain_share, bias_share, expand_share, squeeze_share = jnp.split(
        share, cuts
    )
    return (
        layer_output,
        grad_input,
        mixer_share,
        pre_share[0],
        pre_share[1],
        pre_share[2],
        squeeze_share.reshape(own, RANK),
        expand_share.reshape(-1, RANK).T,
        bias_share,
        pre_share[3],
        head_share,
        output_share.astype(F32),
        feedgain_share,
        gate_share.astype(F32),
        up_share.astype(F32),
        down_share.astype(F32),
    )


def solution(mesh):
    rows = P(BOTH, None)
    spread = P(BOTH)
    in_specs = (
        P("batch", "seq", None),
        P("batch", "seq"),
        spread,
        rows,
        rows,
        rows,
        rows,
        P(None, BOTH),
        spread,
        rows,
        spread,
        rows,
        spread,
        rows,
        rows,
        rows,
        P("batch", "seq", None),
    )
    out_specs = (
        P("batch", "seq", None),
        P("batch", "seq", None),
        spread,
        rows,
        rows,
        rows,
        rows,
        P(None, BOTH),
        spread,
        rows,
        spread,
        rows,
        spread,
        rows,
        rows,
        rows,
    )
    return jax.shard_map(local, mesh=mesh, in_specs=in_specs, out_specs=out_specs, check_vma=False)
```

time: 4070 us -> 1150 us (0.28)
  waiting for transfers between devices: 2780 us -> 683 us
  matrix products: 737 us -> 168 us
  other arithmetic: 177 us -> 51.2 us
  blocking collectives: 165 us -> 46.6 us
    reduce_scatter x8 -> x4, waiting for transfers between devices: 2340 us -> 102 us  [the longest x1 102 us: local(): lax.psum_scatter(term_feedpre, 'batch', scatter_dimension=0, tiled=True)]
    dot_general x133 -> x18, matrix products: 735 us -> 168 us  [the longest x6 59.3 us: dot_nt(): lax.dot_general(left, right, (((1,), (1,)), ((), ())), preferred_element_...]
    unnamed x18 -> x12, waiting for transfers between devices: 5.18 us -> 340 us
    all_gather x8 -> x4, waiting for transfers between devices: 317 us -> 0.01 us  [the longest x1 0.01 us: local(): w_output = lax.all_gather(output_weight, 'batch', axis=0, tiled=True)]
    ppermute x13 -> x36, waiting for transfers between devices: 120 us -> 241 us  [swapped(): return lax.ppermute(block, 'seq', [(i, i ^ by) for i in range(ring)])]
    unnamed x2 -> x0, blocking collectives: 85.9 us -> none
    reduce_sum x18 -> x3, other arithmetic: 68 us -> 4.69 us  [the longest x1 2.93 us: local(): term_feed = jnp.sum(grad_feedin * hidden * scale_two, axis=0)]
  transfers between devices with their start and end apart: 30 -> 46, of which waited for: 23 -> 20; matrix products, arithmetic and copies ran while one was open for 11% -> 17% of each run, Pallas kernels for 0% -> 1%
where the time goes in v1:
time: 1150 us; the launch traced here: 1140 us
  waiting for transfers between devices  683 us (59%)
  matrix products  168 us (15%)
  local copies, waits for them, and re-layouts  96 us (8%)
  other arithmetic  51.2 us (4%)
  blocking collectives  46.6 us (4%)
  starting transfers between devices  44.5 us (4%)
  Pallas kernels  31.7 us (3%)
  between operations  17.3 us (2%)
    unnamed x12, waiting for transfers between devices  340 us
    ppermute x36, waiting for transfers between devices, swapped(): return lax.ppermute(block, 'seq', [(i, i ^ by) for i in range(ring)])  241 us
    reduce_scatter x1, waiting for transfers between devices, local(): lax.psum_scatter(term_feedpre, 'batch', scatter_dimension=0, tiled=True)  102 us
    dot_general x6, matrix products, dot_nt(): lax.dot_general(left, right, (((1,), (1,)), ((), ())), preferred_element_...  59.3 us
    dot_general x6, matrix products, dot_nn(): lax.dot_general(left, right, (((1,), (0,)), ((), ())), preferred_element_...  59.3 us
    dot_general x6, matrix products, dot_tn(): lax.dot_general(left, right, (((0,), (0,)), ((), ())), preferred_element_...  49.8 us
    all_gather x1, blocking collectives, local(): lax.all_gather(segments.reshape(rows), 'seq', axis=0, tiled=True)  46.6 us
    ppermute x36, starting transfers between devices, swapped(): return lax.ppermute(block, 'seq', [(i, i ^ by) for i in range(ring)])  43.9 us
  transfers between devices with their start and end apart: 46, of which 20 were waited for; matrix products, arithmetic and copies ran while one was open for 17% of the time, Pallas kernels for 1%

profile of v1, /device:TPU:0, one launch (start us, length us, event | category | flops | bytes accessed | tf_op | source)
XLA Modules:
  0.0 1138.6 jit_solution(369561324307561095)
XLA Ops:
  13.2 2.2 constant_dynamic-slice_fusion.25
  15.6 4.0 collective-permute-start.5
  22.2 4.5 collective-permute-done.5
  26.7 5.1 collective-permute-done.3
  34.9 3.0 constant_dynamic-slice_fusion.17
  41.7 7.6 collective-permute-done.12
  49.3 7.9 collective-permute-done.13
  64.7 46.6 %all-gather.2 = s32[1,1024]{1,0:T(1,128)S(1)} all-gather(s32[1,256]{1,0:T(1,128)S(1)} %copy-done.62), channel_id=4, replica_groups=mesh['seq'=4,'batch'=8] {'seq'}, dimensions={1}, use_global_device_ids=true | all-gather | bytes 5120 | tf_op jit(solution)/shard_map/all_gather | solution.py:507
  112.9 206.2 %all-reduce.5.cloned.1.call-done = bf16[43264]{0:T(1024)(128)(2,1)} async-done(((bf16[43264]{0:T(1024)(128)(2,1)}), bf16[43264]{0:T(1024)(128)(2,1)}) %all-reduce.5.cloned.1.call-update) | async-done | bytes 86544
  324.8 2.4 fusion.4
  327.3 6.4 fusion.2
  333.7 1.9 copy-done.26
  338.7 12.5 %fusion.58 = (bf16[1024,2048]{1,0:T(8,128)(2,1)S(1)}, f32[1024,2048]{1,0:T(8,128)S(1)}) fusion(bf16[1024,2048]{1,0:T(8,128)(2,1)} %copy-done.26, bf16[2048,2048]{1,0:T(8,128)(2,1)} %bitcast.260), kind=kOutput, calls=%fused_computation.188 | convolution fusion | flops 8592031744 | bytes 25165824 | tf_op jit(solution)/shard_map/dot_general | solution.py:25
  353.6 11.2 mixer_forward.1
  369.2 7.6 fusion.59
  376.8 1.7 fusion.55
  382.1 22.8 %collective-permute-done.6 = bf16[256,2048]{1,0:T(8,128)(2,1)} collective-permute-done((bf16[256,2048]{1,0:T(8,128)(2,1)}, bf16[256,2048]{1,0:T(8,128)(2,1)}, u32[]{:S(2)}, u32[]{:S(2)}) %collective-permute-start.6) | collective-permute-done | bytes 1048608 | tf_op jit(solution)/shard_map/ppermute | solution.py:381
  404.9 23.0 %collective-permute-done.7 = bf16[256,2048]{1,0:T(8,128)(2,1)} collective-permute-done((bf16[256,2048]{1,0:T(8,128)(2,1)}, bf16[256,2048]{1,0:T(8,128)(2,1)}, u32[]{:S(2)}, u32[]{:S(2)}) %collective-permute-start.7) | collective-permute-done | bytes 1048608 | tf_op jit(solution)/shard_map/ppermute | solution.py:381
  427.9 4.3 multiply_reduce_fusion.4
  434.8 2.3 copy.126
  443.9 43.0 %collective-permute-done.10 = bf16[256,2048]{0,1:T(8,128)(2,1)S(1)} collective-permute-done((bf16[256,2048]{0,1:T(8,128)(2,1)S(1)}, bf16[256,2048]{0,1:T(8,128)(2,1)S(1)}, u32[]{:S(2)}, u32[]{:S(2)}) %collective-permute-start.10) | collective-permute-done | bytes 1048608 | tf_op jit(solution)/shard_map/ppermute | solution.py:381
  489.4 20.1 %fusion.29 = f32[1024,2816]{1,0:T(8,128)} fusion(bf16[2048,2816]{1,0:T(8,128)(2,1)} %bitcast.258, bf16[256,2048]{0,1:T(8,128)(2,1)} %copy-done.70, bf16[256,2048]{0,1:T(8,128)(2,1)} %copy-done.68, bf16[256,2048]{0,1:T(8,128)(2,1)} %collective-permute-done.9, bf16[256,2048]{0,1:T(8,128)(2,1)} %bitcast.217), kind=kOutput, calls=%fused_computation.82 | convolution fusion | flops 11827937280 | bytes 27262976 | tf_op jit(solution)/shard_map/dot_general | solution.py:25
  511.0 21.3 %collective-permute-done.20 = bf16[256,2048]{1,0:T(8,128)(2,1)} collective-permute-done((bf16[256,2048]{1,0:T(8,128)(2,1)}, bf16[256,2048]{1,0:T(8,128)(2,1)}, u32[]{:S(2)}, u32[]{:S(2)}) %collective-permute-start.20) | collective-permute-done | bytes 1048608 | tf_op jit(solution)/shard_map/ppermute | solution.py:381
  532.3 17.0 %multiply_convert_fusion.1 = (bf16[1024,1408]{1,0:T(8,128)(2,1)}, bf16[1024,1408]{1,0:T(8,128)(2,1)}, bf16[1024,1408]{1,0:T(8,128)(2,1)}) fusion(f32[1024,2816]{1,0:T(8,128)} %fusion.29, bf16[1408,2048]{1,0:T(8,128)(2,1)} %all-gather.11.cloned.1.call-done, bf16[256,2048]{1,0:T(8,128)(2,1)} %collective-permute-done.20, ...), kind=kOutput, calls=%fused_computation.12 | convolution fusion | flops 5943984128 | bytes 30146560 | tf_op jit(solution)/shard_map/dot_general | solution.py:29
  549.3 19.4 %fusion.60 = (bf16[1024,2048]{1,0:T(8,128)(2,1)}, f32[1024,2048]{1,0:T(8,128)}) fusion(bf16[2048,2816]{1,0:T(8,128)(2,1)} %bitcast.259, bf16[1024,1408]{1,0:T(8,128)(2,1)} %get-tuple-element.93, bf16[1024,1408]{1,0:T(8,128)(2,1)} %get-tuple-element.92), kind=kOutput, calls=%fused_computation.190 | convolution fusion | flops 11824791552 | bytes 29884416 | tf_op jit(solution)/shard_map/dot_general | solution.py:29
  568.8 2.2 fusion.53
  574.6 8.8 fusion.61
  583.4 1.7 fusion.54
  587.4 9.8 collective-permute-done.21
  598.8 21.4 %collective-permute-done.22 = bf16[256,2048]{1,0:T(8,128)(2,1)S(1)} collective-permute-done((bf16[256,2048]{1,0:T(8,128)(2,1)S(1)}, bf16[256,2048]{1,0:T(8,128)(2,1)S(1)}, u32[]{:S(2)}, u32[]{:S(2)}) %collective-permute-start.22) | collective-permute-done | bytes 1048608 | tf_op jit(solution)/shard_map/ppermute | solution.py:381
  620.2 3.6 fusion.14
  623.9 2.9 copy.128
  626.7 3.2 copy.129
  629.9 3.3 copy.130
  633.2 2.9 multiply_reduce_fusion
  636.2 6.1 collective-permute-done.15
  642.2 20.1 %collective-permute-done.16 = bf16[256,2048]{1,0:T(8,128)(2,1)} collective-permute-done((bf16[256,2048]{1,0:T(8,128)(2,1)}, bf16[256,2048]{1,0:T(8,128)(2,1)}, u32[]{:S(2)}, u32[]{:S(2)}) %collective-permute-start.16) | collective-permute-done | bytes 1048608 | tf_op jit(solution)/shard_map/ppermute | solution.py:381
  662.4 5.7 fusion.51
  671.7 22.9 %collective-permute-done.24 = bf16[256,2048]{1,0:T(8,128)(2,1)} collective-permute-done((bf16[256,2048]{1,0:T(8,128)(2,1)}, bf16[256,2048]{1,0:T(8,128)(2,1)}, u32[]{:S(2)}, u32[]{:S(2)}) %collective-permute-start.24) | collective-permute-done | bytes 1048608 | tf_op jit(solution)/shard_map/ppermute | solution.py:381
  694.5 20.2 %collective-permute-done.25 = bf16[256,2048]{1,0:T(8,128)(2,1)} collective-permute-done((bf16[256,2048]{1,0:T(8,128)(2,1)}, bf16[256,2048]{1,0:T(8,128)(2,1)}, u32[]{:S(2)}, u32[]{:S(2)}) %collective-permute-start.25) | collective-permute-done | bytes 1048608 | tf_op jit(solution)/shard_map/ppermute | solution.py:381
  714.8 6.6 multiply_reduce_fusion.1
  721.5 3.7 subtract_convert_fusion
  725.3 20.4 %mixer_backward.1 = (bf16[1024,512]{1,0:T(8,128)(2,1)S(1)}, bf16[1024,512]{1,0:T(8,128)(2,1)S(1)}, bf16[1024,512]{1,0:T(8,128)(2,1)S(1)}, f32[64,1024]{1,0:T(8,128)S(1)}) custom-call(s32[1]{0:T(128)} %bitcast.1.mine, bf16[1024,512]{1,0:T(8,128)(2,1)S(1)} %copy-done.3, bf16[1024,512]{1,0:T(8,128)(2,1)S(1)} %copy-done.1, ...), custom_call_target="tpu_custom_call" | custom-call | flops 2097152000 | bytes 10485760 | tf_op jit(solution)/shard_map/mixer_backward/pallas_call | solution.py:346
  753.5 1.8 reshape.347
  757.9 13.9 %fusion.27 = f32[1024,2048]{1,0:T(8,128)} fusion(bf16[2048,2048]{1,0:T(8,128)(2,1)} %bitcast.261, bf16[1024,512]{1,0:T(8,128)(2,1)} %get-tuple-element.95, bf16[1024,512]{1,0:T(8,128)(2,1)S(1)} %copy-done.25, bf16[1024,512]{1,0:T(8,128)(2,1)S(1)} %get-tuple-element.31, bf16[1024,512]{1,0:T(8,128)(2,1)S(1)} %get-tuple-element.30), kind=kOutput, calls=%fused_computation.80 | convolution fusion | flops 8606711808 | bytes 20971520 | tf_op jit(solution)/shard_map/dot_general | solution.py:29
  771.8 9.5 fusion.3
  782.5 13.9 %convolution_convert_fusion.2 = bf16[2048,2048]{1,0:T(8,128)(2,1)} fusion(bf16[1024,2048]{1,0:T(8,128)(2,1)} %copy-done.26, bf16[1024,512]{1,0:T(8,128)(2,1)} %get-tuple-element.95, bf16[1024,512]{1,0:T(8,128)(2,1)S(1)} %copy-done.25, bf16[1024,512]{1,0:T(8,128)(2,1)S(1)} %get-tuple-element.31, bf16[1024,512]{1,0:T(8,128)(2,1)S(1)} %get-tuple-element.30), kind=kOutput, calls=%fused_computation.9 | convolution fusion | flops 8610906112 | bytes 16777216 | tf_op jit(solution)/shard_map/dot_general | solution.py:33
  797.6 6.4 convolution_convert_fusion.3
  804.1 10.3 convolution_convert_fusion.1
  816.3 17.7 %convolution_convert_fusion = bf16[2048,2816]{1,0:T(8,128)(2,1)} fusion(bf16[1024,1408]{1,0:T(8,128)(2,1)} %get-tuple-element.93, bf16[1024,1408]{1,0:T(8,128)(2,1)} %get-tuple-element.92, bf16[256,2048]{0,1:T(8,128)(2,1)S(1)} %copy-done.71, bf16[256,2048]{0,1:T(8,128)(2,1)S(1)} %copy-done.69, bf16[256,2048]{0,1:T(8,128)(2,1)} %collective-permute-done.9, ...), kind=kOutput, calls=%fused_computation | convolution fusion | flops 11845238784 | bytes 21495808 | tf_op jit(solution)/shard_map/dot_general | solution.py:33
  834.1 3.7 fusion.52
  839.0 2.3 collective-permute-start.29
  841.4 132.8 %all-reduce.7.cloned.1.call-done = f32[32,1352]{1,0:T(8,128)} async-done(((f32[32,1352]{1,0:T(8,128)}), f32[32,1352]{1,0:T(8,128)}) %all-reduce.7.cloned.1.call-update) | async-done | bytes 173072
  979.9 3.6 fusion.12
  983.5 1.9 copy.134
  987.0 3.0 copy.136
  996.4 3.8 fusion.26
  1000.2 1.8 convert_element_type.272
  1002.0 2.4 convert_element_type.281
  1004.7 101.7 %reduce-scatter.9.cloned.1.call-done = bf16[256,2816]{1,0:T(8,128)(2,1)} async-done(((bf16[2048,2816]{1,0:T(8,128)(2,1)}), bf16[256,2816]{1,0:T(8,128)(2,1)}) %reduce-scatter.9.cloned.1.call-update) | async-done | bytes 1441808 | tf_op jit(solution)/shard_map/reduce_scatter | solution.py:569
  1106.5 2.3 constant_dynamic-slice_fusion.4
  1112.4 2.6 reshape.361
  1115.1 2.9 copy.176
  1122.3 4.1 collective-permute-done.34
  (347 shorter events, 109.1 us)
Async XLA Ops:
  8.0 311.0 %all-reduce.5.cloned.1.call-start = ((), (), s32[]{:S(2)}) async-start(), calls=%async_computation.12 | async-start | bytes 176128
  15.6 11.1 collective-permute-start.5
  19.7 12.1 %collective-permute-start.3 = (bf16[64,2048]{1,0:T(8,128)(2,1)S(1)}, bf16[64,2048]{1,0:T(8,128)(2,1)S(1)}, u32[]{:S(2)}, u32[]{:S(2)}) collective-permute-start(bf16[64,2048]{1,0:T(8,128)(2,1)S(1)} %bitcast.234), channel_id=1, source_target_pairs={{0,8},{8,0},{16,24},{24,16},{1,9},{9,1},{17,25},{25,17},{2,10},{10... | collective-permute-start | bytes 786440 | tf_op jit(solution)/shard_map/ppermute | solution.py:381
  20.4 11.4 %collective-permute-start.4 = (bf16[64,2048]{1,0:T(8,128)(2,1)S(1)}, bf16[64,2048]{1,0:T(8,128)(2,1)S(1)}, u32[]{:S(2)}, u32[]{:S(2)}) collective-permute-start(bf16[64,2048]{1,0:T(8,128)(2,1)S(1)} %bitcast.235), channel_id=1, source_target_pairs={{0,16},{8,24},{16,0},{24,8},{1,17},{9,25},{17,1},{25,9},{2,18},{10... | collective-permute-start | bytes 786440 | tf_op jit(solution)/shard_map/ppermute | solution.py:381
  21.9 316.7 %all-gather.13.cloned.1.call-start = ((), (), s32[]{:S(2)}) async-start(), calls=%async_computation.10 | async-start | bytes 9437184 | tf_op jit(solution)/shard_map/all_gather | solution.py:499
  22.0 11.9 %copy-start.45 = (bf16[64,5632]{1,0:T(8,128)(2,1)S(1)}, bf16[64,5632]{1,0:T(8,128)(2,1)}, u32[]{:S(2)}) copy-start(bf16[64,5632]{1,0:T(8,128)(2,1)} %param.37) | copy-start | bytes 2162692
  33.2 336.0 %all-gather.9.cloned.1.call-start = ((), (), s32[]{:S(2)}) async-start(), calls=%async_computation.4 | async-start | bytes 2359296 | tf_op jit(solution)/shard_map/all_gather | solution.py:500
  33.8 455.6 %all-gather.15.cloned.1.call-start = ((), (), s32[]{:S(2)}) async-start(), calls=%async_computation.11 | async-start | bytes 12976128 | tf_op jit(solution)/shard_map/all_gather | solution.py:502
  37.9 11.4 %collective-permute-start.12 = (bf16[64,2816]{1,0:T(8,128)(2,1)S(1)}, bf16[64,2816]{1,0:T(8,128)(2,1)S(1)}, u32[]{:S(2)}, u32[]{:S(2)}) collective-permute-start(bf16[64,2816]{1,0:T(8,128)(2,1)S(1)} %bitcast.227), channel_id=1, source_target_pairs={{0,8},{8,0},{16,24},{24,16},{1,9},{9,1},{17,25},{25,17},{2,10},{10... | collective-permute-start | bytes 1081352 | tf_op jit(solution)/shard_map/ppermute | solution.py:381
  39.5 17.8 %collective-permute-start.13 = (bf16[64,2816]{1,0:T(8,128)(2,1)S(1)}, bf16[64,2816]{1,0:T(8,128)(2,1)S(1)}, u32[]{:S(2)}, u32[]{:S(2)}) collective-permute-start(bf16[64,2816]{1,0:T(8,128)(2,1)S(1)} %bitcast.228), channel_id=1, source_target_pairs={{0,16},{8,24},{16,0},{24,8},{1,17},{9,25},{17,1},{25,9},{2,18},{10... | collective-permute-start | bytes 1081352 | tf_op jit(solution)/shard_map/ppermute | solution.py:381
  41.0 16.2 %collective-permute-start.14 = (bf16[64,2816]{1,0:T(8,128)(2,1)S(1)}, bf16[64,2816]{1,0:T(8,128)(2,1)S(1)}, u32[]{:S(2)}, u32[]{:S(2)}) collective-permute-start(bf16[64,2816]{1,0:T(8,128)(2,1)S(1)} %bitcast.229), channel_id=1, source_target_pairs={{0,24},{8,16},{16,8},{24,0},{1,25},{9,17},{17,9},{25,1},{2,26},{10... | collective-permute-start | bytes 1081352 | tf_op jit(solution)/shard_map/ppermute | solution.py:381
  58.9 473.4 %all-gather.11.cloned.1.call-start = ((), (), s32[]{:S(2)}) async-start(), calls=%async_computation.5 | async-start | bytes 6488064 | tf_op jit(solution)/shard_map/all_gather | solution.py:505
  61.1 272.6 %copy-start.31 = (bf16[256,2048]{1,0:T(8,128)(2,1)}, bf16[256,2048]{1,0:T(8,128)(2,1)S(1)}, u32[]{:S(2)}) copy-start(bf16[256,2048]{1,0:T(8,128)(2,1)S(1)} %copy.119) | copy-start | bytes 3145732
  61.1 263.7 %collective-permute-start = (bf16[256,2048]{1,0:T(8,128)(2,1)S(1)}, bf16[256,2048]{1,0:T(8,128)(2,1)S(1)}, u32[]{:S(2)}, u32[]{:S(2)}) collective-permute-start(bf16[256,2048]{1,0:T(8,128)(2,1)S(1)} %copy.119), channel_id=1, source_target_pairs={{0,8},{8,0},{16,24},{24,16},{1,9},{9,1},{17,25},{25,17},{2,10},{10... | collective-permute-start | bytes 3145736 | tf_op jit(solution)/shard_map/ppermute | solution.py:381
  62.4 262.4 %collective-permute-start.1 = (bf16[256,2048]{1,0:T(8,128)(2,1)S(1)}, bf16[256,2048]{1,0:T(8,128)(2,1)S(1)}, u32[]{:S(2)}, u32[]{:S(2)}) collective-permute-start(bf16[256,2048]{1,0:T(8,128)(2,1)S(1)} %copy.119), channel_id=1, source_target_pairs={{0,16},{8,24},{16,0},{24,8},{1,17},{9,25},{17,1},{25,9},{2,18},{10... | collective-permute-start | bytes 3145736 | tf_op jit(solution)/shard_map/ppermute | solution.py:381
  63.3 261.5 %collective-permute-start.2 = (bf16[256,2048]{1,0:T(8,128)(2,1)S(1)}, bf16[256,2048]{1,0:T(8,128)(2,1)}, u32[]{:S(2)}, u32[]{:S(2)}) collective-permute-start(bf16[256,2048]{1,0:T(8,128)(2,1)S(1)} %copy.119), channel_id=1, source_target_pairs={{0,24},{8,16},{16,8},{24,0},{1,25},{9,17},{17,9},{25,1},{2,26},{10... | collective-permute-start | bytes 3145736 | tf_op jit(solution)/shard_map/ppermute | solution.py:381
  64.6 909.6 %all-reduce.7.cloned.1.call-start = ((), (), s32[]{:S(2)}) async-start(), calls=%async_computation.13 | async-start | bytes 360448
  324.5 12.3 %copy-start.55 = (bf16[256,16]{1,0:T(8,128)(2,1)}, bf16[256,16]{1,0:T(8,128)(2,1)S(1)}, u32[]{:S(2)}) copy-start(bf16[256,16]{1,0:T(8,128)(2,1)S(1)} %reshape.320) | copy-start | bytes 24580
  351.2 16.5 %copy-start.41 = (f32[1024,2048]{1,0:T(8,128)}, f32[1024,2048]{1,0:T(8,128)S(1)}, u32[]{:S(2)}) copy-start(f32[1024,2048]{1,0:T(8,128)S(1)} %get-tuple-element.175) | copy-start | bytes 25165828
  351.5 15.0 %copy-start = (bf16[1024,512]{1,0:T(8,128)(2,1)}, bf16[1024,512]{1,0:T(8,128)(2,1)S(1)}, u32[]{:S(2)}) copy-start(bf16[1024,512]{1,0:T(8,128)(2,1)S(1)} %get-tuple-element.112.key) | copy-start | bytes 3145732
  351.5 15.0 %copy-start.2 = (bf16[1024,512]{1,0:T(8,128)(2,1)}, bf16[1024,512]{1,0:T(8,128)(2,1)S(1)}, u32[]{:S(2)}) copy-start(bf16[1024,512]{1,0:T(8,128)(2,1)S(1)} %get-tuple-element.113.query) | copy-start | bytes 3145732
  378.6 26.3 %collective-permute-start.6 = (bf16[256,2048]{1,0:T(8,128)(2,1)}, bf16[256,2048]{1,0:T(8,128)(2,1)}, u32[]{:S(2)}, u32[]{:S(2)}) collective-permute-start(bf16[256,2048]{1,0:T(8,128)(2,1)} %get-tuple-element.108), channel_id=1, source_target_pairs={{0,8},{8,0},{16,24},{24,16},{1,9},{9,1},{17,25},{25,17},{2,10},{10... | collective-permute-start | bytes 3145736 | tf_op jit(solution)/shard_map/ppermute | solution.py:381
  380.2 47.7 %collective-permute-start.7 = (bf16[256,2048]{1,0:T(8,128)(2,1)}, bf16[256,2048]{1,0:T(8,128)(2,1)}, u32[]{:S(2)}, u32[]{:S(2)}) collective-permute-start(bf16[256,2048]{1,0:T(8,128)(2,1)} %get-tuple-element.110), channel_id=1, source_target_pairs={{0,16},{8,24},{16,0},{24,8},{1,17},{9,25},{17,1},{25,9},{2,18},{10... | collective-permute-start | bytes 3145736 | tf_op jit(solution)/shard_map/ppermute | solution.py:381
  381.4 46.5 %collective-permute-start.8 = (bf16[256,2048]{1,0:T(8,128)(2,1)}, bf16[256,2048]{1,0:T(8,128)(2,1)}, u32[]{:S(2)}, u32[]{:S(2)}) collective-permute-start(bf16[256,2048]{1,0:T(8,128)(2,1)} %get-tuple-element.109), channel_id=1, source_target_pairs={{0,24},{8,16},{16,8},{24,0},{1,25},{9,17},{17,9},{25,1},{2,26},{10... | collective-permute-start | bytes 3145736 | tf_op jit(solution)/shard_map/ppermute | solution.py:381
  438.3 48.6 %collective-permute-start.10 = (bf16[256,2048]{0,1:T(8,128)(2,1)S(1)}, bf16[256,2048]{0,1:T(8,128)(2,1)S(1)}, u32[]{:S(2)}, u32[]{:S(2)}) collective-permute-start(bf16[256,2048]{0,1:T(8,128)(2,1)S(1)} %bitcast.214), channel_id=1, source_target_pairs={{0,16},{8,24},{16,0},{24,8},{1,17},{9,25},{17,1},{25,9},{2,18},{10... | collective-permute-start | bytes 3145736 | tf_op jit(solution)/shard_map/ppermute | solution.py:381
  439.9 48.6 %collective-permute-start.11 = (bf16[256,2048]{0,1:T(8,128)(2,1)S(1)}, bf16[256,2048]{0,1:T(8,128)(2,1)S(1)}, u32[]{:S(2)}, u32[]{:S(2)}) collective-permute-start(bf16[256,2048]{0,1:T(8,128)(2,1)S(1)} %bitcast.215), channel_id=1, source_target_pairs={{0,24},{8,16},{16,8},{24,0},{1,25},{9,17},{17,9},{25,1},{2,26},{10... | collective-permute-start | bytes 3145736 | tf_op jit(solution)/shard_map/ppermute | solution.py:381
  441.0 48.4 %collective-permute-start.9 = (bf16[256,2048]{0,1:T(8,128)(2,1)S(1)}, bf16[256,2048]{0,1:T(8,128)(2,1)}, u32[]{:S(2)}, u32[]{:S(2)}) collective-permute-start(bf16[256,2048]{0,1:T(8,128)(2,1)S(1)} %bitcast.216), channel_id=1, source_target_pairs={{0,8},{8,0},{16,24},{24,16},{1,9},{9,1},{17,25},{25,17},{2,10},{10... | collective-permute-start | bytes 3145736 | tf_op jit(solution)/shard_map/ppermute | solution.py:381
  441.9 69.1 %collective-permute-start.18 = (bf16[256,2048]{1,0:T(8,128)(2,1)}, bf16[256,2048]{1,0:T(8,128)(2,1)}, u32[]{:S(2)}, u32[]{:S(2)}) collective-permute-start(bf16[256,2048]{1,0:T(8,128)(2,1)} %bitcast.208), channel_id=1, source_target_pairs={{0,8},{8,0},{16,24},{24,16},{1,9},{9,1},{17,25},{25,17},{2,10},{10... | collective-permute-start | bytes 3145736 | tf_op jit(solution)/shard_map/ppermute | solution.py:381
  443.1 67.9 %collective-permute-start.19 = (bf16[256,2048]{1,0:T(8,128)(2,1)}, bf16[256,2048]{1,0:T(8,128)(2,1)}, u32[]{:S(2)}, u32[]{:S(2)}) collective-permute-start(bf16[256,2048]{1,0:T(8,128)(2,1)} %bitcast.209), channel_id=1, source_target_pairs={{0,16},{8,24},{16,0},{24,8},{1,17},{9,25},{17,1},{25,9},{2,18},{10... | collective-permute-start | bytes 3145736 | tf_op jit(solution)/shard_map/ppermute | solution.py:381
  487.0 45.3 %collective-permute-start.20 = (bf16[256,2048]{1,0:T(8,128)(2,1)}, bf16[256,2048]{1,0:T(8,128)(2,1)}, u32[]{:S(2)}, u32[]{:S(2)}) collective-permute-start(bf16[256,2048]{1,0:T(8,128)(2,1)} %bitcast.210), channel_id=1, source_target_pairs={{0,24},{8,16},{16,8},{24,0},{1,25},{9,17},{17,9},{25,1},{2,26},{10... | collective-permute-start | bytes 3145736 | tf_op jit(solution)/shard_map/ppermute | solution.py:381
  549.3 25.2 %copy-start.72 = (bf16[1024,1408]{1,0:T(8,128)(2,1)S(1)}, bf16[1024,1408]{1,0:T(8,128)(2,1)}, u32[]{:S(2)}) copy-start(bf16[1024,1408]{1,0:T(8,128)(2,1)} %get-tuple-element.96) | copy-start | bytes 8650756
  571.0 26.2 %collective-permute-start.21 = (bf16[256,2048]{1,0:T(8,128)(2,1)S(1)}, bf16[256,2048]{1,0:T(8,128)(2,1)S(1)}, u32[]{:S(2)}, u32[]{:S(2)}) collective-permute-start(bf16[256,2048]{1,0:T(8,128)(2,1)S(1)} %get-tuple-element.102), channel_id=1, source_target_pairs={{0,8},{8,0},{16,24},{24,16},{1,9},{9,1},{17,25},{25,17},{2,10},{10... | collective-permute-start | bytes 3145736 | tf_op jit(solution)/shard_map/ppermute | solution.py:381
  571.6 48.6 %collective-permute-start.22 = (bf16[256,2048]{1,0:T(8,128)(2,1)S(1)}, bf16[256,2048]{1,0:T(8,128)(2,1)S(1)}, u32[]{:S(2)}, u32[]{:S(2)}) collective-permute-start(bf16[256,2048]{1,0:T(8,128)(2,1)S(1)} %get-tuple-element.104), channel_id=1, source_target_pairs={{0,16},{8,24},{16,0},{24,8},{1,17},{9,25},{17,1},{25,9},{2,18},{10... | collective-permute-start | bytes 3145736 | tf_op jit(solution)/shard_map/ppermute | solution.py:381
  573.3 46.9 %collective-permute-start.23 = (bf16[256,2048]{1,0:T(8,128)(2,1)S(1)}, bf16[256,2048]{1,0:T(8,128)(2,1)S(1)}, u32[]{:S(2)}, u32[]{:S(2)}) collective-permute-start(bf16[256,2048]{1,0:T(8,128)(2,1)S(1)} %get-tuple-element.103), channel_id=1, source_target_pairs={{0,24},{8,16},{16,8},{24,0},{1,25},{9,17},{17,9},{25,1},{2,26},{10... | collective-permute-start | bytes 3145736 | tf_op jit(solution)/shard_map/ppermute | solution.py:381
  585.1 57.1 %collective-permute-start.15 = (bf16[256,2048]{1,0:T(8,128)(2,1)}, bf16[256,2048]{1,0:T(8,128)(2,1)}, u32[]{:S(2)}, u32[]{:S(2)}) collective-permute-start(bf16[256,2048]{1,0:T(8,128)(2,1)} %get-tuple-element.105), channel_id=1, source_target_pairs={{0,8},{8,0},{16,24},{24,16},{1,9},{9,1},{17,25},{25,17},{2,10},{10... | collective-permute-start | bytes 3145736 | tf_op jit(solution)/shard_map/ppermute | solution.py:381
  585.7 76.6 %collective-permute-start.16 = (bf16[256,2048]{1,0:T(8,128)(2,1)}, bf16[256,2048]{1,0:T(8,128)(2,1)}, u32[]{:S(2)}, u32[]{:S(2)}) collective-permute-start(bf16[256,2048]{1,0:T(8,128)(2,1)} %get-tuple-element.107), channel_id=1, source_target_pairs={{0,16},{8,24},{16,0},{24,8},{1,17},{9,25},{17,1},{25,9},{2,18},{10... | collective-permute-start | bytes 3145736 | tf_op jit(solution)/shard_map/ppermute | solution.py:381
  597.2 65.2 %collective-permute-start.17 = (bf16[256,2048]{1,0:T(8,128)(2,1)}, bf16[256,2048]{1,0:T(8,128)(2,1)}, u32[]{:S(2)}, u32[]{:S(2)}) collective-permute-start(bf16[256,2048]{1,0:T(8,128)(2,1)} %get-tuple-element.106), channel_id=1, source_target_pairs={{0,24},{8,16},{16,8},{24,0},{1,25},{9,17},{17,9},{25,1},{2,26},{10... | collective-permute-start | bytes 3145736 | tf_op jit(solution)/shard_map/ppermute | solution.py:381
  633.2 29.1 %copy-start.29 = (f32[256,2048]{1,0:T(8,128)S(1)}, f32[256,2048]{1,0:T(8,128)}, u32[]{:S(2)}) copy-start(f32[256,2048]{1,0:T(8,128)} %copy-done.28) | copy-start | bytes 6291460
  633.2 29.1 %copy-start.30 = (f32[256,2048]{1,0:T(8,128)S(1)}, f32[256,2048]{1,0:T(8,128)}, u32[]{:S(2)}) copy-start(f32[256,2048]{1,0:T(8,128)} %copy.130) | copy-start | bytes 6291460
  668.1 26.4 %collective-permute-start.24 = (bf16[256,2048]{1,0:T(8,128)(2,1)}, bf16[256,2048]{1,0:T(8,128)(2,1)}, u32[]{:S(2)}, u32[]{:S(2)}) collective-permute-start(bf16[256,2048]{1,0:T(8,128)(2,1)} %get-tuple-element.88), channel_id=1, source_target_pairs={{0,8},{8,0},{16,24},{24,16},{1,9},{9,1},{17,25},{25,17},{2,10},{10... | collective-permute-start | bytes 3145736 | tf_op jit(solution)/shard_map/ppermute | solution.py:381
  669.6 45.2 %collective-permute-start.25 = (bf16[256,2048]{1,0:T(8,128)(2,1)}, bf16[256,2048]{1,0:T(8,128)(2,1)}, u32[]{:S(2)}, u32[]{:S(2)}) collective-permute-start(bf16[256,2048]{1,0:T(8,128)(2,1)} %get-tuple-element.88), channel_id=1, source_target_pairs={{0,16},{8,24},{16,0},{24,8},{1,17},{9,25},{17,1},{25,9},{2,18},{10... | collective-permute-start | bytes 3145736 | tf_op jit(solution)/shard_map/ppermute | solution.py:381
  670.2 44.6 %collective-permute-start.26 = (bf16[256,2048]{1,0:T(8,128)(2,1)}, bf16[256,2048]{1,0:T(8,128)(2,1)}, u32[]{:S(2)}, u32[]{:S(2)}) collective-permute-start(bf16[256,2048]{1,0:T(8,128)(2,1)} %get-tuple-element.88), channel_id=1, source_target_pairs={{0,24},{8,16},{16,8},{24,0},{1,25},{9,17},{17,9},{25,1},{2,26},{10... | collective-permute-start | bytes 3145736 | tf_op jit(solution)/shard_map/ppermute | solution.py:381
  725.3 21.5 %copy-start.50 = (f32[64,1024]{1,0:T(8,128)S(1)}, f32[64,1024]{1,0:T(8,128)}, u32[]{:S(2)}) copy-start(f32[64,1024]{1,0:T(8,128)} %get-tuple-element.176) | copy-start | bytes 786436
  725.3 22.6 %copy-start.27 = (bf16[1024,2048]{1,0:T(8,128)(2,1)S(1)}, bf16[1024,2048]{1,0:T(8,128)(2,1)}, u32[]{:S(2)}) copy-start(bf16[1024,2048]{1,0:T(8,128)(2,1)} %copy-done.26) | copy-start | bytes 12582916
  747.9 9.9 copy-start.25
  757.8 13.9 %copy-start.32 = (bf16[256,2048]{1,0:T(8,128)(2,1)S(1)}, bf16[256,2048]{1,0:T(8,128)(2,1)}, u32[]{:S(2)}) copy-start(bf16[256,2048]{1,0:T(8,128)(2,1)} %copy-done.31) | copy-start | bytes 3145732
  757.8 13.9 %copy-start.34 = (bf16[256,2048]{1,0:T(8,128)(2,1)S(1)}, bf16[256,2048]{1,0:T(8,128)(2,1)}, u32[]{:S(2)}) copy-start(bf16[256,2048]{1,0:T(8,128)(2,1)} %copy-done.33) | copy-start | bytes 3145732
  757.8 13.9 %copy-start.36 = (bf16[256,2048]{1,0:T(8,128)(2,1)S(1)}, bf16[256,2048]{1,0:T(8,128)(2,1)}, u32[]{:S(2)}) copy-start(bf16[256,2048]{1,0:T(8,128)(2,1)} %copy-done.35) | copy-start | bytes 3145732
  757.8 13.9 %copy-start.48 = (bf16[16,2048]{1,0:T(8,128)(2,1)S(1)}, bf16[16,2048]{1,0:T(8,128)(2,1)}, u32[]{:S(2)}) copy-start(bf16[16,2048]{1,0:T(8,128)(2,1)} %copy-done.47) | copy-start | bytes 196612
  757.9 13.9 %copy-start.58 = (f32[1024]{0:T(1024)S(1)}, f32[1024]{0:T(1024)}, u32[]{:S(2)}) copy-start(f32[1024]{0:T(1024)} %copy-done.57) | copy-start | bytes 12292
  782.5 209.1 %reduce-scatter.5.cloned.1.call-start = ((), (), s32[]{:S(2)}) async-start(), calls=%async_computation.6 | async-start | bytes 9437184 | tf_op jit(solution)/shard_map/reduce_scatter | solution.py:620
  796.4 203.8 %reduce-scatter.7.cloned.1.call-start = ((), (), s32[]{:S(2)}) async-start(), calls=%async_computation.7 | async-start | bytes 2359296 | tf_op jit(solution)/shard_map/reduce_scatter | solution.py:584
  804.0 198.0 %reduce-scatter.11.cloned.1.call-start = ((), (), s32[]{:S(2)}) async-start(), calls=%async_computation.9 | async-start | bytes 6488064 | tf_op jit(solution)/shard_map/reduce_scatter | solution.py:568
  814.4 292.0 %reduce-scatter.9.cloned.1.call-start = ((), (), s32[]{:S(2)}) async-start(), calls=%async_computation.8 | async-start | bytes 12976128 | tf_op jit(solution)/shard_map/reduce_scatter | solution.py:569
  837.8 142.1 %collective-permute-start.27 = (bf16[256,2048]{1,0:T(8,128)(2,1)}, bf16[256,2048]{1,0:T(8,128)(2,1)S(1)}, u32[]{:S(2)}, u32[]{:S(2)}) collective-permute-start(bf16[256,2048]{1,0:T(8,128)(2,1)} %get-tuple-element.99), channel_id=1, source_target_pairs={{0,8},{8,0},{16,24},{24,16},{1,9},{9,1},{17,25},{25,17},{2,10},{10... | collective-permute-start | bytes 3145736 | tf_op jit(solution)/shard_map/ppermute | solution.py:381
  837.8 142.1 %collective-permute-start.28 = (bf16[256,2048]{1,0:T(8,128)(2,1)}, bf16[256,2048]{1,0:T(8,128)(2,1)S(1)}, u32[]{:S(2)}, u32[]{:S(2)}) collective-permute-start(bf16[256,2048]{1,0:T(8,128)(2,1)} %get-tuple-element.101), channel_id=1, source_target_pairs={{0,16},{8,24},{16,0},{24,8},{1,17},{9,25},{17,1},{25,9},{2,18},{10... | collective-permute-start | bytes 3145736 | tf_op jit(solution)/shard_map/ppermute | solution.py:381
  839.0 141.0 %collective-permute-start.29 = (bf16[256,2048]{1,0:T(8,128)(2,1)}, bf16[256,2048]{1,0:T(8,128)(2,1)S(1)}, u32[]{:S(2)}, u32[]{:S(2)}) collective-permute-start(bf16[256,2048]{1,0:T(8,128)(2,1)} %get-tuple-element.100), channel_id=1, source_target_pairs={{0,24},{8,16},{16,8},{24,0},{1,25},{9,17},{17,9},{25,1},{2,26},{10... | collective-permute-start | bytes 3145736 | tf_op jit(solution)/shard_map/ppermute | solution.py:381
  987.0 9.5 copy-start.38
  992.9 11.5 %collective-permute-start.30 = (bf16[64,2048]{1,0:T(8,128)(2,1)S(1)}, bf16[64,2048]{1,0:T(8,128)(2,1)S(1)}, u32[]{:S(2)}, u32[]{:S(2)}) collective-permute-start(bf16[64,2048]{1,0:T(8,128)(2,1)S(1)} %get-tuple-element.144), channel_id=1, source_target_pairs={{0,8},{8,0},{16,24},{24,16},{1,9},{9,1},{17,25},{25,17},{2,10},{10... | collective-permute-start | bytes 786440 | tf_op jit(solution)/shard_map/ppermute | solution.py:381
  994.6 9.9 collective-permute-start.31
  996.1 8.4 collective-permute-start.32
  1108.8 13.5 %collective-permute-start.33 = (bf16[64,2816]{1,0:T(8,128)(2,1)}, bf16[64,2816]{1,0:T(8,128)(2,1)}, u32[]{:S(2)}, u32[]{:S(2)}) collective-permute-start(bf16[64,2816]{1,0:T(8,128)(2,1)} %get-tuple-element.128), channel_id=1, source_target_pairs={{0,8},{8,0},{16,24},{24,16},{1,9},{9,1},{17,25},{25,17},{2,10},{10... | collective-permute-start | bytes 1081352 | tf_op jit(solution)/shard_map/ppermute | solution.py:381
  1110.2 16.1 %collective-permute-start.34 = (bf16[64,2816]{1,0:T(8,128)(2,1)}, bf16[64,2816]{1,0:T(8,128)(2,1)}, u32[]{:S(2)}, u32[]{:S(2)}) collective-permute-start(bf16[64,2816]{1,0:T(8,128)(2,1)} %get-tuple-element.127), channel_id=1, source_target_pairs={{0,16},{8,24},{16,0},{24,8},{1,17},{9,25},{17,1},{25,9},{2,18},{10... | collective-permute-start | bytes 1081352 | tf_op jit(solution)/shard_map/ppermute | solution.py:381
  1111.7 14.7 %collective-permute-start.35 = (bf16[64,2816]{1,0:T(8,128)(2,1)}, bf16[64,2816]{1,0:T(8,128)(2,1)}, u32[]{:S(2)}, u32[]{:S(2)}) collective-permute-start(bf16[64,2816]{1,0:T(8,128)(2,1)} %get-tuple-element.126), channel_id=1, source_target_pairs={{0,24},{8,16},{16,8},{24,0},{1,25},{9,17},{17,9},{25,1},{2,26},{10... | collective-permute-start | bytes 1081352 | tf_op jit(solution)/shard_map/ppermute | solution.py:381
  (55 other events, 212.6 us)
Sparse Core Ops, SparseCore 0:
  22.1 296.9 all-reduce.4
  782.6 191.5 all-reduce.6
Sparse Core Ops, SparseCore 1:
  33.3 83.2 all-gather.12
  118.0 27.8 all-gather.8
  148.0 107.6 all-gather.14
  257.3 58.7 all-gather.10
  796.5 86.9 reduce-scatter.4
  885.7 34.3 reduce-scatter.6
  922.3 64.6 reduce-scatter.10
  989.1 117.3 reduce-scatter.8

commit v2 on v1

--- a/solution.py
+++ b/solution.py
@@ -382,15 +382,61 @@
 
 
 def gathered(block, ring):
-    return jnp.concatenate([block] + [swapped(block, by, ring) for by in range(1, ring)], axis=0)
+    if ring != 4:
+        return jnp.concatenate([block] + [swapped(block, by, ring) for by in range(1, ring)], axis=0)
+    half = block.shape[0] // 2
+    one, two = swapped(block, 1, ring), swapped(block, 2, ring)
+    low, high = swapped(two[:half], 1, ring), swapped(one[half:], 2, ring)
+    return jnp.concatenate([block, one, two, low, high], axis=0)
 
 
 def scattered(terms, ring):
     rows = terms.shape[0] // ring
-    total = terms[:rows].astype(F32)
-    for by in range(1, ring):
-        total = total + swapped(terms[by * rows : (by + 1) * rows].astype(BF16), by, ring).astype(F32)
-    return total
+    parts = [terms[by * rows : (by + 1) * rows] for by in range(ring)]
+    total = parts[0].astype(F32)
+    if ring != 4:
+        for by in range(1, ring):
+            total = total + swapped(parts[by], by, ring).astype(F32)
+        return total
+    half = rows // 2
+    low, high = swapped(parts[3][:half], 1, ring), swapped(parts[3][half:], 2, ring)
+    two = jnp.concatenate([added(parts[2][:half], low), parts[2][half:]], axis=0)
+    one = jnp.concatenate([parts[1][:half], added(parts[1][half:], high)], axis=0)
+    return total + swapped(one, 1, ring).astype(F32) + swapped(two, 2, ring).astype(F32)
+
+
+def added(left, right):
+    return (left.astype(F32) + right.astype(F32)).astype(BF16)
+
+
+def flipped(block, axis, by):
+    return lax.ppermute(block, axis, [(i, i ^ by) for i in range(lax.axis_size(axis))])
+
+
+def doubled(block, axis):
+    by, mine = 1, lax.axis_index(axis)
+    while by < lax.axis_size(axis):
+        other = flipped(block, axis, by)
+        first = (mine & by) == 0
+        block = jnp.concatenate(
+            [jnp.where(first, block, other), jnp.where(first, other, block)], axis=0
+        )
+        by *= 2
+    return block
+
+
+def halved(block, axis):
+    by, mine = lax.axis_size(axis) // 2, lax.axis_index(axis)
+    while by:
+        low, high = jnp.split(block, 2, axis=0)
+        first = (mine & by) == 0
+        block = jnp.where(first, low, high) + flipped(jnp.where(first, high, low), axis, by)
+        by //= 2
+    return block
+
+
+def after(value, *others):
+    return lax.optimization_barrier((value,) + others)[0]
 
 
 def exchanged(blocks, mine, ring):
@@ -476,7 +522,7 @@
             squeeze.reshape(-1),
         ]
     )
-    small = lax.all_gather(small, BOTH, axis=0, tiled=False)
+    small = doubled(doubled(small[None], "batch"), "seq")
     cuts = np.cumsum([own, own, own, slots_all // devices, RANK * slots_all // devices])
     gain_one, gain_head, gain_two, bias_full, expand_t, w_squeeze = jnp.split(small, cuts, axis=1)
     gain_one = permuted(gain_one.reshape(width)).astype(F32)
@@ -504,7 +550,7 @@
     )
     w_down = lax.all_gather(down_weight, "batch", axis=0, tiled=True)
 
-    segment = lax.all_gather(segments.reshape(rows), "seq", axis=0, tiled=True).astype(F32)
+    segment = doubled(segments.reshape(1, rows), "seq").reshape(length).astype(F32)
     chunked = segment.reshape(-1, CHUNK)
     before = jnp.concatenate([jnp.full((1,), -1.0, F32), chunked[:-1, -1]])
     previous = jnp.concatenate([jnp.full((1,), -1.0, F32), segment[:-1]])
@@ -520,7 +566,10 @@
     segment_col = segment[:, None]
 
     input_own = layer_input.reshape(rows, width)
-    inputs = gathered(permuted(input_own), ring).astype(F32)
+    inputs = gathered(permuted(input_own), ring)
+    grad_own = cotangent.reshape(rows, width)
+    grad_out = gathered(after(grad_own, inputs), ring)
+    inputs = inputs.astype(F32)
     scale_one = rms_scale(inputs)
     plain_one = inputs * scale_one
     normed = (plain_one * gain_one).astype(BF16)
@@ -543,7 +592,7 @@
     swish_sig = jax.nn.sigmoid(swish_pre)
     swish_act = swish_pre * swish_sig
     gated = own_part((head_normed * swish_act).astype(BF16))
-    hidden = input_own.astype(F32) + scattered(dot_nn(gated, w_output), ring)
+    hidden = input_own.astype(F32) + scattered(dot_nn(gated, w_output).astype(BF16), ring)
 
     scale_two = rms_scale(hidden)
     feed_in = gathered(permuted((hidden * scale_two * gain_two).astype(BF16)), ring)
@@ -552,21 +601,21 @@
     gate_sig = jax.nn.sigmoid(gate_pre)
     gate_act = gate_pre * gate_sig
     inner = (gate_act * up_pre).astype(BF16)
-    result = hidden + scattered(dot_nn(inner, w_down), ring)
-    layer_output = result.astype(BF16).reshape(1, rows, width)
-
-    grad_own = cotangent.reshape(rows, width)
-    grad_out = gathered(grad_own, ring)
-    grad_inner = dot_nt(grad_out, w_down)
+
+    term_down = dot_tn(inner, grad_out).astype(BF16)
+    grad_inner = dot_nt(after(grad_out, term_down), w_down)
     grad_gatepre = grad_inner * up_pre * (gate_sig * (1.0 + gate_pre * (1.0 - gate_sig)))
     grad_feedpre = jnp.concatenate(
         [grad_gatepre.astype(BF16), (grad_inner * gate_act).astype(BF16)], axis=1
     )
-    grad_feedin = restored(scattered(dot_nt(grad_feedpre, w_feed), ring))
-    term_down = dot_tn(inner, grad_out).astype(BF16)
-    term_feedpre = dot_tn(feed_in, grad_feedpre).astype(BF16)
+    back_feedin = dot_nt(grad_feedpre, w_feed).astype(BF16)
+    grad_feedin = restored(scattered(back_feedin, ring))
+    term_feedpre = dot_tn(feed_in, after(grad_feedpre, back_feedin)).astype(BF16)
+    result = hidden + scattered(dot_nn(after(inner, term_feedpre), w_down).astype(BF16), ring)
+    layer_output = result.astype(BF16).reshape(1, rows, width)
     down_share = lax.psum_scatter(term_down, "batch", scatter_dimension=0, tiled=True)
-    feed_share = lax.psum_scatter(term_feedpre, "batch", scatter_dimension=0, tiled=True)
+    feed_share = lax.psum_scatter(after(term_feedpre, down_share), "batch", scatter_dimension=0, tiled=True)
+    feed_sum = feed_share
     feed_share = exchanged(feed_share.reshape(ring, own, 2 * hidden_part), mine, ring)
     gate_share = feed_share[:, :, :hidden_part].transpose(1, 0, 2).reshape(own, -1)
     up_share = feed_share[:, :, hidden_part:].transpose(1, 0, 2).reshape(own, -1)
@@ -578,10 +627,9 @@
         - hidden * scale_two**3 * jnp.mean(scaled_two * hidden, axis=-1, keepdims=True)
     )
 
-    grad_branch = gathered(grad_hidden.astype(BF16), ring)
+    grad_branch = after(gathered(grad_hidden.astype(BF16), ring), term_feedpre)
     grad_gated = whole_head(dot_nt(grad_branch, w_output))
     term_output = dot_tn(gated, grad_branch).astype(BF16)
-    output_share = lax.psum_scatter(term_output, "batch", scatter_dimension=0, tiled=True)
     slope = swish_sig * (1.0 + swish_pre * (1.0 - swish_sig))
     grad_swishpre = own_part((grad_gated * head_normed * slope).astype(BF16))
     grad_normed_head = grad_gated * swish_act
@@ -615,9 +663,12 @@
     grad_normed = dot_nt(grad_pre, w_mixer) + dot_nn(grad_reduced, w_squeeze)
     term_mixer = restored(jnp.sum(grad_normed * plain_one, axis=0))
     term_squeeze = restored(dot_tn(grad_reduced, normed))
-    grad_normed = restored(scattered(grad_normed, ring))
     term_pre = dot_tn(normed, grad_pre).astype(BF16)
-    pre_share = lax.psum_scatter(term_pre, "batch", scatter_dimension=0, tiled=True)
+    grad_normed = restored(scattered(after(grad_normed.astype(BF16), term_pre), ring))
+    pre_share = lax.psum_scatter(after(term_pre, feed_sum), "batch", scatter_dimension=0, tiled=True)
+    output_share = lax.psum_scatter(
+        after(term_output, pre_share), "batch", scatter_dimension=0, tiled=True
+    )
     pre_share = exchanged(pre_share.reshape(ring, own, 4 * part), mine, ring)
     pre_share = pre_share.reshape(ring, own, 4, part).transpose(2, 1, 0, 3).reshape(4, own, width)
     pre_share = pre_share.astype(F32)
@@ -646,7 +697,7 @@
         ],
         axis=1,
     )
-    share = lax.psum_scatter(terms, BOTH, scatter_dimension=0, tiled=True)[0]
+    share = halved(halved(terms, "seq"), "batch")[0]
     mixer_share, head_share, feedgain_share, bias_share, expand_share, squeeze_share = jnp.split(
         share, cuts
     )

time: 1150 us -> 694 us (0.60)
  waiting for transfers between devices: 683 us -> 256 us
  blocking collectives: 46.6 us -> 0 us
  starting transfers between devices: 44.5 us -> 65.4 us
  local copies, waits for them, and re-layouts: 96 us -> 114 us
  matrix products: 168 us -> 153 us
    unnamed x12 -> x8, waiting for transfers between devices: 340 us -> 0.81 us
    reduce_scatter x3, waiting for transfers between devices: 102 us -> 0.02 us  [the longest x1 0.02 us: local(): lax.psum_scatter(after(term_pre, feed_sum), 'batch', scatter_dimension=0,...]
    ppermute x36 -> x44, waiting for transfers between devices: 241 us -> 194 us  [swapped(): return lax.ppermute(block, 'seq', [(i, i ^ by) for i in range(ring)])]
    all_gather x1 -> x0, blocking collectives: 46.6 us -> none  [local(): lax.all_gather(segments.reshape(rows), 'seq', axis=0, tiled=True)]
    ppermute x0 -> x12, waiting for transfers between devices: none -> 41.9 us  [flipped(): lax.ppermute(block, axis, [(i, i ^ by) for i in range(lax.axis_size(axis))])]
    unnamed x169 -> x191, local copies, waits for them, and re-layouts: 22.7 us -> 41.9 us
    ppermute x0 -> x12, starting transfers between devices: none -> 15.8 us  [flipped(): lax.ppermute(block, axis, [(i, i ^ by) for i in range(lax.axis_size(axis))])]
    ppermute x36 -> x44, starting transfers between devices: 43.9 us -> 49 us  [swapped(): return lax.ppermute(block, 'seq', [(i, i ^ by) for i in range(ring)])]
  transfers between devices with their start and end apart: 46 -> 64, of which waited for: 20 -> 41; matrix products, arithmetic and copies ran while one was open for 17% -> 42% of each run, Pallas kernels for 1% -> 5%
where the time goes in v2:
time: 694 us; the launch traced here: 685 us
  waiting for transfers between devices  256 us (37%)
  matrix products  153 us (22%)
  local copies, waits for them, and re-layouts  114 us (16%)
  starting transfers between devices  65.4 us (9%)
  other arithmetic  48.1 us (7%)
  Pallas kernels  31.6 us (5%)
  between operations  16.2 us (2%)
    ppermute x44, waiting for transfers between devices, swapped(): return lax.ppermute(block, 'seq', [(i, i ^ by) for i in range(ring)])  194 us
    dot_general x6, matrix products, dot_nt(): lax.dot_general(left, right, (((1,), (1,)), ((), ())), preferred_element_...  53.1 us
    dot_general x6, matrix products, dot_nn(): lax.dot_general(left, right, (((1,), (0,)), ((), ())), preferred_element_...  51.6 us
    ppermute x44, starting transfers between devices, swapped(): return lax.ppermute(block, 'seq', [(i, i ^ by) for i in range(ring)])  49 us
    dot_general x6, matrix products, dot_tn(): lax.dot_general(left, right, (((0,), (0,)), ((), ())), preferred_element_...  48.2 us
    ppermute x12, waiting for transfers between devices, flipped(): lax.ppermute(block, axis, [(i, i ^ by) for i in range(lax.axis_size(axis))])  41.9 us
    unnamed x191, local copies, waits for them, and re-layouts  41.9 us
    pallas_call x1, Pallas kernels, mixer_backward(): pl.pallas_call(kernel, out_shape=(jax.ShapeDtypeStruct((length, size), BF...  20.6 us
  transfers between devices with their start and end apart: 64, of which 41 were waited for; matrix products, arithmetic and copies ran while one was open for 42% of the time, Pallas kernels for 5%

profile of v2, /device:TPU:0, one launch (start us, length us, event | category | flops | bytes accessed | tf_op | source)
XLA Modules:
  0.0 684.9 jit_solution(2188894705301606856)
XLA Ops:
  14.7 4.0 collective-permute-start.11
  19.8 6.0 collective-permute-done.11
  25.8 5.0 collective-permute-done.9
  34.0 3.0 constant_dynamic-slice_fusion.17
  40.9 7.6 %collective-permute-done.22 = bf16[64,2816]{1,0:T(8,128)(2,1)S(1)} collective-permute-done((bf16[64,2816]{1,0:T(8,128)(2,1)S(1)}, bf16[64,2816]{1,0:T(8,128)(2,1)S(1)}, u32[]{:S(2)}, u32[]{:S(2)}) %collective-permute-start.22) | collective-permute-done | bytes 360480 | tf_op jit(solution)/shard_map/ppermute | solution.py:381
  48.4 8.0 %collective-permute-done.23 = bf16[64,2816]{1,0:T(8,128)(2,1)S(1)} collective-permute-done((bf16[64,2816]{1,0:T(8,128)(2,1)S(1)}, bf16[64,2816]{1,0:T(8,128)(2,1)S(1)}, u32[]{:S(2)}, u32[]{:S(2)}) %collective-permute-start.23) | collective-permute-done | bytes 360480 | tf_op jit(solution)/shard_map/ppermute | solution.py:381
  65.0 18.9 %collective-permute-done.12 = s32[1,256]{1,0:T(1,128)S(1)} collective-permute-done((s32[1,256]{1,0:T(1,128)S(1)}, s32[1,256]{1,0:T(1,128)S(1)}, u32[]{:S(2)}, u32[]{:S(2)}) %collective-permute-start.12) | collective-permute-done | bytes 1056 | tf_op jit(solution)/shard_map/ppermute | solution.py:413
  87.6 4.2 collective-permute-done.5
  92.2 4.6 collective-permute-done.6
  97.1 3.6 collective-permute-done.7
  101.3 3.5 collective-permute-done.8
  111.3 2.3 constant_dynamic-update-slice_fusion.3
  113.6 2.3 constant_dynamic-update-slice_fusion.2
  119.8 3.2 fusion.4
  125.6 12.6 %fusion.45 = (bf16[1024,2048]{1,0:T(8,128)(2,1)S(1)}, f32[1024,2048]{1,0:T(8,128)S(1)}) fusion(bf16[2048,2048]{1,0:T(8,128)(2,1)} %bitcast.261, bf16[1024,2048]{1,0:T(8,128)(2,1)} %constant_dynamic-update-slice_fusion, f32[2048]{0:T(1024)S(1)} %reshape.427, f32[1024]{0:T(1024)S(1)} %add_rsqrt_fusion.1), kind=kOutput, calls=%fused_computation.241 | convolution fusion | flops 8600420352 | bytes 25178112 | tf_op jit(solution)/shard_map/dot_general | solution.py:25
  139.8 11.1 %mixer_forward.1 = (f32[1024,512]{1,0:T(8,128)S(1)}, f32[64,1024]{1,0:T(8,128)S(1)}, f32[64,1024]{1,0:T(8,128)S(1)}, f32[8,64,512]{2,1,0:T(8,128)S(1)}, f32[8,64,512]{2,1,0:T(8,128)S(1)}) custom-call(s32[1]{0:T(128)} %bitcast.1.mine, bf16[1024,512]{1,0:T(8,128)(2,1)S(1)} %get-tuple-element.143.query, bf16[1024,512]{1,0:T(8,128)(2,1)S(1)} %get-tuple-element.142.key, ...), custom_call_target="tpu_custom_call" | custom-call | flops 1048576000 | bytes 6291456 | tf_op jit(solution)/shard_map/mixer_forward/pallas_call | solution.py:311
  154.6 4.7 convolution_convert_fusion.5
  163.6 10.9 %collective-permute-done.14 = bf16[128,2048]{1,0:T(8,128)(2,1)S(1)} collective-permute-done((bf16[128,2048]{1,0:T(8,128)(2,1)S(1)}, bf16[128,2048]{1,0:T(8,128)(2,1)S(1)}, u32[]{:S(2)}, u32[]{:S(2)}) %collective-permute-start.14) | collective-permute-done | bytes 524320 | tf_op jit(solution)/shard_map/ppermute | solution.py:381
  181.1 16.0 %collective-permute-done.26 = bf16[256,2048]{1,0:T(8,128)(2,1)} collective-permute-done((bf16[256,2048]{1,0:T(8,128)(2,1)}, bf16[256,2048]{1,0:T(8,128)(2,1)}, u32[]{:S(2)}, u32[]{:S(2)}) %collective-permute-start.26) | collective-permute-done | bytes 1048608 | tf_op jit(solution)/shard_map/ppermute | solution.py:381
  202.5 8.3 %collective-permute-done.17 = bf16[256,2048]{1,0:T(8,128)(2,1)} collective-permute-done((bf16[256,2048]{1,0:T(8,128)(2,1)}, bf16[256,2048]{1,0:T(8,128)(2,1)}, u32[]{:S(2)}, u32[]{:S(2)}) %collective-permute-start.17) | collective-permute-done | bytes 1048608 | tf_op jit(solution)/shard_map/ppermute | solution.py:381
  210.8 3.5 multiply_reduce_fusion.4
  216.9 10.3 %copy.123 = bf16[256,2048]{0,1:T(8,128)(2,1)} copy(bf16[256,2048]{1,0:T(8,128)(2,1)} %multiply_convert_fusion.4) | data formatting | bytes 2097152 | tf_op jit(solution)/shard_map/convert_element_type | solution.py:598
  237.3 24.0 %collective-permute-done.28 = bf16[128,2048]{1,0:T(8,128)(2,1)S(1)} collective-permute-done((bf16[128,2048]{1,0:T(8,128)(2,1)S(1)}, bf16[128,2048]{1,0:T(8,128)(2,1)S(1)}, u32[]{:S(2)}, u32[]{:S(2)}) %collective-permute-start.28) | collective-permute-done | bytes 524320 | tf_op jit(solution)/shard_map/ppermute | solution.py:381
  266.3 4.3 collective-permute-done.20
  273.0 18.3 %fusion.46 = f32[1024,2816]{1,0:T(8,128)S(1)} fusion(bf16[1024,2048]{0,1:T(8,128)(2,1)} %constant_dynamic-update-slice_fusion.9, bf16[2048,2816]{1,0:T(8,128)(2,1)} %bitcast.259), kind=kOutput, calls=%fused_computation.242 | convolution fusion | flops 11811160064 | bytes 27262976 | tf_op jit(solution)/shard_map/dot_general | solution.py:25
  293.2 3.6 copy-done.29
  298.3 8.1 %convolution_convert_fusion.2 = bf16[1408,2048]{1,0:T(8,128)(2,1)} fusion(bf16[1024,1408]{1,0:T(8,128)(2,1)S(1)} %multiply_convert_fusion.2, bf16[1024,2048]{1,0:T(8,128)(2,1)S(1)} %copy-done.55), kind=kOutput, calls=%fused_computation.9 | convolution fusion | flops 5908463616 | bytes 12845056 | tf_op jit(solution)/shard_map/dot_general | solution.py:33
  306.5 8.8 %all-gather.9.cloned.1.call-done = bf16[1408,2048]{1,0:T(8,128)(2,1)} async-done(((bf16[176,2048]{1,0:T(8,128)(2,1)}), bf16[1408,2048]{1,0:T(8,128)(2,1)}) %all-gather.9.cloned.1.call-update) | async-done | bytes 5767184 | tf_op jit(solution)/shard_map/all_gather | solution.py:551
  315.3 15.6 %multiply_convert_fusion.1 = (bf16[1024,1408]{1,0:T(8,128)(2,1)S(1)}, bf16[1024,1408]{1,0:T(8,128)(2,1)}) fusion(f32[1024,2816]{1,0:T(8,128)} %copy-done.29, bf16[1024,2048]{1,0:T(8,128)(2,1)} %copy-done.54, bf16[1408,2048]{1,0:T(8,128)(2,1)} %all-gather.9.cloned.1.call-done), kind=kOutput, calls=%fused_computation.12 | convolution fusion | flops 5924323328 | bytes 27262976 | tf_op jit(solution)/shard_map/dot_general | solution.py:29
  334.6 18.1 %convolution_convert_fusion.3 = bf16[1024,2048]{1,0:T(8,128)(2,1)} fusion(bf16[2048,2816]{1,0:T(8,128)(2,1)} %bitcast.260, bf16[1024,1408]{1,0:T(8,128)(2,1)} %get-tuple-element.112, bf16[1024,1408]{1,0:T(8,128)(2,1)} %copy-done.40), kind=kOutput, calls=%fused_computation.18 | convolution fusion | flops 11824791552 | bytes 21495808 | tf_op jit(solution)/shard_map/dot_general | solution.py:29
  352.7 17.5 %convolution_convert_fusion = bf16[2048,2816]{1,0:T(8,128)(2,1)} fusion(bf16[1024,2048]{0,1:T(8,128)(2,1)} %constant_dynamic-update-slice_fusion.9, bf16[1024,2816]{1,0:T(8,128)(2,1)S(1)} %pad_maximum_fusion), kind=kOutput, calls=%fused_computation | convolution fusion | flops 11816927232 | bytes 21495808 | tf_op jit(solution)/shard_map/dot_general | solution.py:33
  370.2 10.8 %reduce-scatter.5.cloned.1.call-done = bf16[176,2048]{1,0:T(8,128)(2,1)} async-done(((bf16[1408,2048]{1,0:T(8,128)(2,1)}), bf16[176,2048]{1,0:T(8,128)(2,1)}) %reduce-scatter.5.cloned.1.call-update) | async-done | bytes 720912 | tf_op jit(solution)/shard_map/reduce_scatter | solution.py:616
  386.0 9.8 %convolution_convert_fusion.4 = bf16[1024,2048]{1,0:T(8,128)(2,1)S(1)} fusion(bf16[1024,1408]{1,0:T(8,128)(2,1)S(1)} %copy-done.39, bf16[1408,2048]{1,0:T(8,128)(2,1)} %all-gather.9.cloned.1.call-done), kind=kOutput, calls=%fused_computation.19 | convolution fusion | flops 5907677184 | bytes 12845056 | tf_op jit(solution)/shard_map/dot_general | solution.py:25
  396.5 3.1 copy-done.35
  400.9 10.1 %collective-permute-done.29 = bf16[128,2048]{1,0:T(8,128)(2,1)S(1)} collective-permute-done((bf16[128,2048]{1,0:T(8,128)(2,1)S(1)}, bf16[128,2048]{1,0:T(8,128)(2,1)S(1)}, u32[]{:S(2)}, u32[]{:S(2)}) %collective-permute-start.29) | collective-permute-done | bytes 524320 | tf_op jit(solution)/shard_map/ppermute | solution.py:381
  415.5 18.0 %collective-permute-done.34 = bf16[256,2048]{1,0:T(8,128)(2,1)S(1)} collective-permute-done((bf16[256,2048]{1,0:T(8,128)(2,1)S(1)}, bf16[256,2048]{1,0:T(8,128)(2,1)S(1)}, u32[]{:S(2)}, u32[]{:S(2)}) %collective-permute-start.34) | collective-permute-done | bytes 1048608 | tf_op jit(solution)/shard_map/ppermute | solution.py:381
  435.4 2.9 copy.125
  438.3 3.2 copy.126
  441.5 2.9 copy.127
  444.4 7.7 %collective-permute-done.30 = bf16[256,2048]{1,0:T(8,128)(2,1)} collective-permute-done((bf16[256,2048]{1,0:T(8,128)(2,1)}, bf16[256,2048]{1,0:T(8,128)(2,1)}, u32[]{:S(2)}, u32[]{:S(2)}) %collective-permute-start.30) | collective-permute-done | bytes 1048608 | tf_op jit(solution)/shard_map/ppermute | solution.py:381
  452.1 5.3 multiply_reduce_fusion
  457.4 3.5 constant_dynamic-update-slice_fusion.25
  462.8 19.5 %collective-permute-done.38 = bf16[256,2048]{1,0:T(8,128)(2,1)S(1)} collective-permute-done((bf16[256,2048]{1,0:T(8,128)(2,1)S(1)}, bf16[256,2048]{1,0:T(8,128)(2,1)S(1)}, u32[]{:S(2)}, u32[]{:S(2)}) %collective-permute-start.38) | collective-permute-done | bytes 1048608 | tf_op jit(solution)/shard_map/ppermute | solution.py:381
  482.3 3.0 collective-permute-start.39
  486.7 7.8 %collective-permute-done.39 = bf16[128,2048]{1,0:T(8,128)(2,1)S(1)} collective-permute-done((bf16[128,2048]{1,0:T(8,128)(2,1)S(1)}, bf16[128,2048]{1,0:T(8,128)(2,1)S(1)}, u32[]{:S(2)}, u32[]{:S(2)}) %collective-permute-start.39) | collective-permute-done | bytes 524320 | tf_op jit(solution)/shard_map/ppermute | solution.py:381
  495.0 3.1 multiply_reduce_fusion.1
  501.1 20.6 %mixer_backward.1 = (bf16[1024,512]{1,0:T(8,128)(2,1)S(1)}, bf16[1024,512]{1,0:T(8,128)(2,1)S(1)}, bf16[1024,512]{1,0:T(8,128)(2,1)S(1)}, f32[64,1024]{1,0:T(8,128)S(1)}) custom-call(s32[1]{0:T(128)} %bitcast.1.mine, bf16[1024,512]{1,0:T(8,128)(2,1)S(1)} %copy-done.5, bf16[1024,512]{1,0:T(8,128)(2,1)S(1)} %copy-done.3, bf16[1024,512]{1,0:T(8,128)(2,1)S(1)} %copy-done.1, ...), custom_call_target="tpu_custom_call" | custom-call | flops 2097152000 | bytes 10485760 | tf_op jit(solution)/shard_map/mixer_backward/pallas_call | solution.py:346
  523.0 12.3 %convolution_convert_fusion.1 = bf16[2048,2048]{1,0:T(8,128)(2,1)} fusion(bf16[1024,512]{1,0:T(8,128)(2,1)S(1)} %get-tuple-element.114, bf16[1024,512]{1,0:T(8,128)(2,1)S(1)} %get-tuple-element.46, bf16[1024,512]{1,0:T(8,128)(2,1)S(1)} %get-tuple-element.45, bf16[1024,512]{1,0:T(8,128)(2,1)S(1)} %get-tuple-element.44, bf16[1024,2048]{1,0:T(8,128)(2,1)S(1)} %copy-done.26, ...), kind=kOutput, calls=%fused_computation.8 | convolution fusion | flops 8619294720 | bytes 16789504 | tf_op jit(solution)/shard_map/dot_general | solution.py:33
  537.3 3.5 fusion.33
  545.8 2.6 reshape.421
  548.7 14.0 %fusion.16 = f32[1024,2048]{1,0:T(8,128)} fusion(bf16[2048,2048]{1,0:T(8,128)(2,1)} %bitcast.262, bf16[1024,512]{1,0:T(8,128)(2,1)} %copy-done.42, bf16[1024,512]{1,0:T(8,128)(2,1)S(1)} %copy-done.22, bf16[1024,512]{1,0:T(8,128)(2,1)S(1)} %copy-done.20, bf16[1024,512]{1,0:T(8,128)(2,1)S(1)} %get-tuple-element.44), kind=kOutput, calls=%fused_computation.83 | convolution fusion | flops 8606711808 | bytes 20971520 | tf_op jit(solution)/shard_map/dot_general | solution.py:29
  562.7 6.0 fusion.3
  570.6 3.3 collective-permute-done.45
  575.5 2.6 collective-permute-done.46
  578.1 7.8 %collective-permute-start.47 = (f32[4,1352]{1,0:T(4,128)S(1)}, f32[4,1352]{1,0:T(4,128)S(1)}, u32[]{:S(2)}, u32[]{:S(2)}) collective-permute-start(f32[4,1352]{1,0:T(4,128)S(1)} %slice_select_fusion.2), channel_id=1, source_target_pairs={{0,4},{1,5},{2,6},{3,7},{4,0},{5,1},{6,2},{7,3},{8,12},{9,13},{10,... | collective-permute-start | bytes 64904 | tf_op jit(solution)/shard_map/ppermute | solution.py:413
  585.9 6.0 convolution_convert_fusion.6
  596.2 7.4 %collective-permute-done.41 = bf16[128,2048]{1,0:T(8,128)(2,1)S(1)} collective-permute-done((bf16[128,2048]{1,0:T(8,128)(2,1)S(1)}, bf16[128,2048]{1,0:T(8,128)(2,1)S(1)}, u32[]{:S(2)}, u32[]{:S(2)}) %collective-permute-start.41) | collective-permute-done | bytes 524320 | tf_op jit(solution)/shard_map/ppermute | solution.py:381
  611.8 14.3 %collective-permute-done.42 = bf16[256,2048]{1,0:T(8,128)(2,1)S(1)} collective-permute-done((bf16[256,2048]{1,0:T(8,128)(2,1)S(1)}, bf16[256,2048]{1,0:T(8,128)(2,1)S(1)}, u32[]{:S(2)}, u32[]{:S(2)}) %collective-permute-start.42) | collective-permute-done | bytes 1048608 | tf_op jit(solution)/shard_map/ppermute | solution.py:381
  627.7 3.0 convert_add_fusion.1
  645.0 2.3 collective-permute-done.53
  647.3 4.9 collective-permute-done.54
  661.6 4.2 collective-permute-done.51
  666.2 2.4 reshape.432
  668.7 2.9 copy.177
  (452 shorter events, 165.9 us)
Async XLA Ops:
  7.2 118.4 %all-gather.11.cloned.1.call-start = ((), (), s32[]{:S(2)}) async-start(), calls=%async_computation.10 | async-start | bytes 9437184 | tf_op jit(solution)/shard_map/all_gather | solution.py:545
  14.7 11.1 %collective-permute-start.11 = (bf16[64,2048]{1,0:T(8,128)(2,1)S(1)}, bf16[64,2048]{1,0:T(8,128)(2,1)S(1)}, u32[]{:S(2)}, u32[]{:S(2)}) collective-permute-start(bf16[64,2048]{1,0:T(8,128)(2,1)S(1)} %bitcast.235), channel_id=1, source_target_pairs={{0,24},{8,16},{16,8},{24,0},{1,25},{9,17},{17,9},{25,1},{2,26},{10... | collective-permute-start | bytes 786440 | tf_op jit(solution)/shard_map/ppermute | solution.py:381
  18.8 12.1 %collective-permute-start.9 = (bf16[64,2048]{1,0:T(8,128)(2,1)S(1)}, bf16[64,2048]{1,0:T(8,128)(2,1)S(1)}, u32[]{:S(2)}, u32[]{:S(2)}) collective-permute-start(bf16[64,2048]{1,0:T(8,128)(2,1)S(1)} %bitcast.236), channel_id=1, source_target_pairs={{0,8},{8,0},{16,24},{24,16},{1,9},{9,1},{17,25},{25,17},{2,10},{10... | collective-permute-start | bytes 786440 | tf_op jit(solution)/shard_map/ppermute | solution.py:381
  19.5 11.3 %collective-permute-start.10 = (bf16[64,2048]{1,0:T(8,128)(2,1)S(1)}, bf16[64,2048]{1,0:T(8,128)(2,1)S(1)}, u32[]{:S(2)}, u32[]{:S(2)}) collective-permute-start(bf16[64,2048]{1,0:T(8,128)(2,1)S(1)} %bitcast.237), channel_id=1, source_target_pairs={{0,16},{8,24},{16,0},{24,8},{1,17},{9,25},{17,1},{25,9},{2,18},{10... | collective-permute-start | bytes 786440 | tf_op jit(solution)/shard_map/ppermute | solution.py:381
  32.2 122.3 %all-gather.7.cloned.1.call-start = ((), (), s32[]{:S(2)}) async-start(), calls=%async_computation.4 | async-start | bytes 2359296 | tf_op jit(solution)/shard_map/all_gather | solution.py:546
  33.0 240.0 %all-gather.13.cloned.1.call-start = ((), (), s32[]{:S(2)}) async-start(), calls=%async_computation.11 | async-start | bytes 12976128 | tf_op jit(solution)/shard_map/all_gather | solution.py:548
  37.1 11.4 %collective-permute-start.22 = (bf16[64,2816]{1,0:T(8,128)(2,1)S(1)}, bf16[64,2816]{1,0:T(8,128)(2,1)S(1)}, u32[]{:S(2)}, u32[]{:S(2)}) collective-permute-start(bf16[64,2816]{1,0:T(8,128)(2,1)S(1)} %bitcast.224), channel_id=1, source_target_pairs={{0,8},{8,0},{16,24},{24,16},{1,9},{9,1},{17,25},{25,17},{2,10},{10... | collective-permute-start | bytes 1081352 | tf_op jit(solution)/shard_map/ppermute | solution.py:381
  38.7 17.7 %collective-permute-start.23 = (bf16[64,2816]{1,0:T(8,128)(2,1)S(1)}, bf16[64,2816]{1,0:T(8,128)(2,1)S(1)}, u32[]{:S(2)}, u32[]{:S(2)}) collective-permute-start(bf16[64,2816]{1,0:T(8,128)(2,1)S(1)} %bitcast.225), channel_id=1, source_target_pairs={{0,16},{8,24},{16,0},{24,8},{1,17},{9,25},{17,1},{25,9},{2,18},{10... | collective-permute-start | bytes 1081352 | tf_op jit(solution)/shard_map/ppermute | solution.py:381
  40.2 16.2 %collective-permute-start.24 = (bf16[64,2816]{1,0:T(8,128)(2,1)S(1)}, bf16[64,2816]{1,0:T(8,128)(2,1)S(1)}, u32[]{:S(2)}, u32[]{:S(2)}) collective-permute-start(bf16[64,2816]{1,0:T(8,128)(2,1)S(1)} %bitcast.226), channel_id=1, source_target_pairs={{0,24},{8,16},{16,8},{24,0},{1,25},{9,17},{17,9},{25,1},{2,26},{10... | collective-permute-start | bytes 1081352 | tf_op jit(solution)/shard_map/ppermute | solution.py:381
  58.1 257.2 %all-gather.9.cloned.1.call-start = ((), (), s32[]{:S(2)}) async-start(), calls=%async_computation.5 | async-start | bytes 6488064 | tf_op jit(solution)/shard_map/all_gather | solution.py:551
  59.7 48.9 %collective-permute-start = (bf16[256,2048]{1,0:T(8,128)(2,1)S(1)}, bf16[256,2048]{1,0:T(8,128)(2,1)}, u32[]{:S(2)}, u32[]{:S(2)}) collective-permute-start(bf16[256,2048]{1,0:T(8,128)(2,1)S(1)} %copy.116), channel_id=1, source_target_pairs={{0,8},{8,0},{16,24},{24,16},{1,9},{9,1},{17,25},{25,17},{2,10},{10... | collective-permute-start | bytes 3145736 | tf_op jit(solution)/shard_map/ppermute | solution.py:381
  60.9 44.6 %collective-permute-start.1 = (bf16[256,2048]{1,0:T(8,128)(2,1)S(1)}, bf16[256,2048]{1,0:T(8,128)(2,1)}, u32[]{:S(2)}, u32[]{:S(2)}) collective-permute-start(bf16[256,2048]{1,0:T(8,128)(2,1)S(1)} %copy.116), channel_id=1, source_target_pairs={{0,16},{8,24},{16,0},{24,8},{1,17},{9,25},{17,1},{25,9},{2,18},{10... | collective-permute-start | bytes 3145736 | tf_op jit(solution)/shard_map/ppermute | solution.py:381
  62.2 23.3 %collective-permute-start.4 = (bf16[1,1352]{1,0:T(2,128)(2,1)S(1)}, bf16[1,1352]{1,0:T(2,128)(2,1)S(1)}, u32[]{:S(2)}, u32[]{:S(2)}) collective-permute-start(bf16[1,1352]{1,0:T(2,128)(2,1)S(1)} %broadcast_in_dim.14), channel_id=1, source_target_pairs={{0,1},{1,0},{2,3},{3,2},{4,5},{5,4},{6,7},{7,6},{8,9},{9,8},{10,11... | collective-permute-start | bytes 8120 | tf_op jit(solution)/shard_map/ppermute | solution.py:413
  62.3 21.6 %collective-permute-start.12 = (s32[1,256]{1,0:T(1,128)S(1)}, s32[1,256]{1,0:T(1,128)S(1)}, u32[]{:S(2)}, u32[]{:S(2)}) collective-permute-start(s32[1,256]{1,0:T(1,128)S(1)} %copy-done.68), channel_id=1, source_target_pairs={{0,8},{8,0},{16,24},{24,16},{1,9},{9,1},{17,25},{25,17},{2,10},{10... | collective-permute-start | bytes 3080 | tf_op jit(solution)/shard_map/ppermute | solution.py:413
  83.9 3.6 collective-permute-start.13
  85.5 6.3 collective-permute-start.5
  91.9 4.9 collective-permute-start.6
  96.8 3.9 collective-permute-start.7
  100.7 4.1 collective-permute-start.8
  107.4 9.5 %collective-permute-start.2 = (bf16[128,2048]{1,0:T(8,128)(2,1)}, bf16[128,2048]{1,0:T(8,128)(2,1)}, u32[]{:S(2)}, u32[]{:S(2)}) collective-permute-start(bf16[128,2048]{1,0:T(8,128)(2,1)} %slice.253), channel_id=1, source_target_pairs={{0,8},{8,0},{16,24},{24,16},{1,9},{9,1},{17,25},{25,17},{2,10},{10... | collective-permute-start | bytes 1572872 | tf_op jit(solution)/shard_map/ppermute | solution.py:381
  109.7 9.2 %collective-permute-start.3 = (bf16[128,2048]{1,0:T(8,128)(2,1)S(1)}, bf16[128,2048]{1,0:T(8,128)(2,1)S(1)}, u32[]{:S(2)}, u32[]{:S(2)}) collective-permute-start(bf16[128,2048]{1,0:T(8,128)(2,1)S(1)} %slice.254), channel_id=1, source_target_pairs={{0,16},{8,24},{16,0},{24,8},{1,17},{9,25},{17,1},{25,9},{2,18},{10... | collective-permute-start | bytes 1572872 | tf_op jit(solution)/shard_map/ppermute | solution.py:381
  159.5 14.9 %collective-permute-start.14 = (bf16[128,2048]{1,0:T(8,128)(2,1)S(1)}, bf16[128,2048]{1,0:T(8,128)(2,1)S(1)}, u32[]{:S(2)}, u32[]{:S(2)}) collective-permute-start(bf16[128,2048]{1,0:T(8,128)(2,1)S(1)} %get-tuple-element.138), channel_id=1, source_target_pairs={{0,16},{8,24},{16,0},{24,8},{1,17},{9,25},{17,1},{25,9},{2,18},{10... | collective-permute-start | bytes 1572872 | tf_op jit(solution)/shard_map/ppermute | solution.py:381
  161.0 13.6 %collective-permute-start.16 = (bf16[128,2048]{1,0:T(8,128)(2,1)S(1)}, bf16[128,2048]{1,0:T(8,128)(2,1)S(1)}, u32[]{:S(2)}, u32[]{:S(2)}) collective-permute-start(bf16[128,2048]{1,0:T(8,128)(2,1)S(1)} %get-tuple-element.137), channel_id=1, source_target_pairs={{0,8},{8,0},{16,24},{24,16},{1,9},{9,1},{17,25},{25,17},{2,10},{10... | collective-permute-start | bytes 1572872 | tf_op jit(solution)/shard_map/ppermute | solution.py:381
  161.6 35.4 %collective-permute-start.26 = (bf16[256,2048]{1,0:T(8,128)(2,1)}, bf16[256,2048]{1,0:T(8,128)(2,1)}, u32[]{:S(2)}, u32[]{:S(2)}) collective-permute-start(bf16[256,2048]{1,0:T(8,128)(2,1)} %bitcast.27), channel_id=1, source_target_pairs={{0,16},{8,24},{16,0},{24,8},{1,17},{9,25},{17,1},{25,9},{2,18},{10... | collective-permute-start | bytes 3145736 | tf_op jit(solution)/shard_map/ppermute | solution.py:381
  176.0 26.4 %collective-permute-start.15 = (bf16[256,2048]{1,0:T(8,128)(2,1)}, bf16[256,2048]{1,0:T(8,128)(2,1)}, u32[]{:S(2)}, u32[]{:S(2)}) collective-permute-start(bf16[256,2048]{1,0:T(8,128)(2,1)} %pad_maximum_fusion.8), channel_id=1, source_target_pairs={{0,8},{8,0},{16,24},{24,16},{1,9},{9,1},{17,25},{25,17},{2,10},{10... | collective-permute-start | bytes 3145736 | tf_op jit(solution)/shard_map/ppermute | solution.py:381
  178.9 31.9 %collective-permute-start.17 = (bf16[256,2048]{1,0:T(8,128)(2,1)}, bf16[256,2048]{1,0:T(8,128)(2,1)}, u32[]{:S(2)}, u32[]{:S(2)}) collective-permute-start(bf16[256,2048]{1,0:T(8,128)(2,1)} %pad_maximum_fusion.9), channel_id=1, source_target_pairs={{0,16},{8,24},{16,0},{24,8},{1,17},{9,25},{17,1},{25,9},{2,18},{10... | collective-permute-start | bytes 3145736 | tf_op jit(solution)/shard_map/ppermute | solution.py:381
  180.9 200.1 %reduce-scatter.5.cloned.1.call-start = ((), (), s32[]{:S(2)}) async-start(), calls=%async_computation.6 | async-start | bytes 6488064 | tf_op jit(solution)/shard_map/reduce_scatter | solution.py:616
  181.0 50.4 %collective-permute-start.25 = (bf16[256,2048]{1,0:T(8,128)(2,1)}, bf16[256,2048]{1,0:T(8,128)(2,1)}, u32[]{:S(2)}, u32[]{:S(2)}) collective-permute-start(bf16[256,2048]{1,0:T(8,128)(2,1)} %bitcast.27), channel_id=1, source_target_pairs={{0,8},{8,0},{16,24},{24,16},{1,9},{9,1},{17,25},{25,17},{2,10},{10... | collective-permute-start | bytes 3145736 | tf_op jit(solution)/shard_map/ppermute | solution.py:381
  198.9 37.3 %collective-permute-start.27 = (bf16[128,2048]{1,0:T(8,128)(2,1)}, bf16[128,2048]{1,0:T(8,128)(2,1)}, u32[]{:S(2)}, u32[]{:S(2)}) collective-permute-start(bf16[128,2048]{1,0:T(8,128)(2,1)} %slice.270), channel_id=1, source_target_pairs={{0,8},{8,0},{16,24},{24,16},{1,9},{9,1},{17,25},{25,17},{2,10},{10... | collective-permute-start | bytes 1572872 | tf_op jit(solution)/shard_map/ppermute | solution.py:381
  228.5 32.8 %collective-permute-start.19 = (bf16[256,2048]{0,1:T(8,128)(2,1)S(1)}, bf16[256,2048]{0,1:T(8,128)(2,1)S(1)}, u32[]{:S(2)}, u32[]{:S(2)}) collective-permute-start(bf16[256,2048]{0,1:T(8,128)(2,1)S(1)} %bitcast.199), channel_id=1, source_target_pairs={{0,16},{8,24},{16,0},{24,8},{1,17},{9,25},{17,1},{25,9},{2,18},{10... | collective-permute-start | bytes 3145736 | tf_op jit(solution)/shard_map/ppermute | solution.py:381
  232.5 28.8 %collective-permute-start.28 = (bf16[128,2048]{1,0:T(8,128)(2,1)S(1)}, bf16[128,2048]{1,0:T(8,128)(2,1)S(1)}, u32[]{:S(2)}, u32[]{:S(2)}) collective-permute-start(bf16[128,2048]{1,0:T(8,128)(2,1)S(1)} %slice.271), channel_id=1, source_target_pairs={{0,16},{8,24},{16,0},{24,8},{1,17},{9,25},{17,1},{25,9},{2,18},{10... | collective-permute-start | bytes 1572872 | tf_op jit(solution)/shard_map/ppermute | solution.py:381
  233.1 29.7 %collective-permute-start.18 = (bf16[256,2048]{0,1:T(8,128)(2,1)S(1)}, bf16[256,2048]{0,1:T(8,128)(2,1)S(1)}, u32[]{:S(2)}, u32[]{:S(2)}) collective-permute-start(bf16[256,2048]{0,1:T(8,128)(2,1)S(1)} %bitcast.200), channel_id=1, source_target_pairs={{0,8},{8,0},{16,24},{24,16},{1,9},{9,1},{17,25},{25,17},{2,10},{10... | collective-permute-start | bytes 3145736 | tf_op jit(solution)/shard_map/ppermute | solution.py:381
  261.4 9.2 %collective-permute-start.20 = (bf16[128,2048]{0,1:T(8,128)(2,1)S(1)}, bf16[128,2048]{0,1:T(8,128)(2,1)S(1)}, u32[]{:S(2)}, u32[]{:S(2)}) collective-permute-start(bf16[128,2048]{0,1:T(8,128)(2,1)S(1)} %slice.266), channel_id=1, source_target_pairs={{0,8},{8,0},{16,24},{24,16},{1,9},{9,1},{17,25},{25,17},{2,10},{10... | collective-permute-start | bytes 1572872 | tf_op jit(solution)/shard_map/ppermute | solution.py:381
  262.8 9.2 %collective-permute-start.21 = (bf16[128,2048]{0,1:T(8,128)(2,1)S(1)}, bf16[128,2048]{0,1:T(8,128)(2,1)S(1)}, u32[]{:S(2)}, u32[]{:S(2)}) collective-permute-start(bf16[128,2048]{0,1:T(8,128)(2,1)S(1)} %slice.267), channel_id=1, source_target_pairs={{0,16},{8,24},{16,0},{24,8},{1,17},{9,25},{17,1},{25,9},{2,18},{10... | collective-permute-start | bytes 1572872 | tf_op jit(solution)/shard_map/ppermute | solution.py:381
  306.4 228.9 %reduce-scatter.7.cloned.1.call-start = ((), (), s32[]{:S(2)}) async-start(), calls=%async_computation.7 | async-start | bytes 12976128 | tf_op jit(solution)/shard_map/reduce_scatter | solution.py:617
  381.1 252.0 %reduce-scatter.9.cloned.1.call-start = ((), (), s32[]{:S(2)}) async-start(), calls=%async_computation.8 | async-start | bytes 9437184 | tf_op jit(solution)/shard_map/reduce_scatter | solution.py:668
  383.0 13.4 %collective-permute-start.33 = (bf16[128,2048]{1,0:T(8,128)(2,1)S(1)}, bf16[128,2048]{1,0:T(8,128)(2,1)S(1)}, u32[]{:S(2)}, u32[]{:S(2)}) collective-permute-start(bf16[128,2048]{1,0:T(8,128)(2,1)S(1)} %get-tuple-element.126), channel_id=1, source_target_pairs={{0,16},{8,24},{16,0},{24,8},{1,17},{9,25},{17,1},{25,9},{2,18},{10... | collective-permute-start | bytes 1572872 | tf_op jit(solution)/shard_map/ppermute | solution.py:381
  384.6 11.9 %collective-permute-start.35 = (bf16[128,2048]{1,0:T(8,128)(2,1)S(1)}, bf16[128,2048]{1,0:T(8,128)(2,1)S(1)}, u32[]{:S(2)}, u32[]{:S(2)}) collective-permute-start(bf16[128,2048]{1,0:T(8,128)(2,1)S(1)} %get-tuple-element.125), channel_id=1, source_target_pairs={{0,8},{8,0},{16,24},{24,16},{1,9},{9,1},{17,25},{25,17},{2,10},{10... | collective-permute-start | bytes 1572872 | tf_op jit(solution)/shard_map/ppermute | solution.py:381
  396.0 14.9 %collective-permute-start.29 = (bf16[128,2048]{1,0:T(8,128)(2,1)S(1)}, bf16[128,2048]{1,0:T(8,128)(2,1)S(1)}, u32[]{:S(2)}, u32[]{:S(2)}) collective-permute-start(bf16[128,2048]{1,0:T(8,128)(2,1)S(1)} %get-tuple-element.132), channel_id=1, source_target_pairs={{0,16},{8,24},{16,0},{24,8},{1,17},{9,25},{17,1},{25,9},{2,18},{10... | collective-permute-start | bytes 1572872 | tf_op jit(solution)/shard_map/ppermute | solution.py:381
  396.1 15.0 %collective-permute-start.31 = (bf16[128,2048]{1,0:T(8,128)(2,1)S(1)}, bf16[128,2048]{1,0:T(8,128)(2,1)S(1)}, u32[]{:S(2)}, u32[]{:S(2)}) collective-permute-start(bf16[128,2048]{1,0:T(8,128)(2,1)S(1)} %get-tuple-element.131), channel_id=1, source_target_pairs={{0,8},{8,0},{16,24},{24,16},{1,9},{9,1},{17,25},{25,17},{2,10},{10... | collective-permute-start | bytes 1572872 | tf_op jit(solution)/shard_map/ppermute | solution.py:381
  400.1 33.4 %collective-permute-start.34 = (bf16[256,2048]{1,0:T(8,128)(2,1)S(1)}, bf16[256,2048]{1,0:T(8,128)(2,1)S(1)}, u32[]{:S(2)}, u32[]{:S(2)}) collective-permute-start(bf16[256,2048]{1,0:T(8,128)(2,1)S(1)} %pad_maximum_fusion.12), channel_id=1, source_target_pairs={{0,8},{8,0},{16,24},{24,16},{1,9},{9,1},{17,25},{25,17},{2,10},{10... | collective-permute-start | bytes 3145736 | tf_op jit(solution)/shard_map/ppermute | solution.py:381
  400.3 33.3 %collective-permute-start.36 = (bf16[256,2048]{1,0:T(8,128)(2,1)S(1)}, bf16[256,2048]{1,0:T(8,128)(2,1)S(1)}, u32[]{:S(2)}, u32[]{:S(2)}) collective-permute-start(bf16[256,2048]{1,0:T(8,128)(2,1)S(1)} %pad_maximum_fusion.13), channel_id=1, source_target_pairs={{0,16},{8,24},{16,0},{24,8},{1,17},{9,25},{17,1},{25,9},{2,18},{10... | collective-permute-start | bytes 3145736 | tf_op jit(solution)/shard_map/ppermute | solution.py:381
  412.5 39.5 %collective-permute-start.30 = (bf16[256,2048]{1,0:T(8,128)(2,1)}, bf16[256,2048]{1,0:T(8,128)(2,1)}, u32[]{:S(2)}, u32[]{:S(2)}) collective-permute-start(bf16[256,2048]{1,0:T(8,128)(2,1)} %pad_maximum_fusion.10), channel_id=1, source_target_pairs={{0,8},{8,0},{16,24},{24,16},{1,9},{9,1},{17,25},{25,17},{2,10},{10... | collective-permute-start | bytes 3145736 | tf_op jit(solution)/shard_map/ppermute | solution.py:381
  413.9 38.2 %collective-permute-start.32 = (bf16[256,2048]{1,0:T(8,128)(2,1)}, bf16[256,2048]{1,0:T(8,128)(2,1)}, u32[]{:S(2)}, u32[]{:S(2)}) collective-permute-start(bf16[256,2048]{1,0:T(8,128)(2,1)} %pad_maximum_fusion.11), channel_id=1, source_target_pairs={{0,16},{8,24},{16,0},{24,8},{1,17},{9,25},{17,1},{25,9},{2,18},{10... | collective-permute-start | bytes 3145736 | tf_op jit(solution)/shard_map/ppermute | solution.py:381
  460.9 21.4 %collective-permute-start.38 = (bf16[256,2048]{1,0:T(8,128)(2,1)S(1)}, bf16[256,2048]{1,0:T(8,128)(2,1)S(1)}, u32[]{:S(2)}, u32[]{:S(2)}) collective-permute-start(bf16[256,2048]{1,0:T(8,128)(2,1)S(1)} %get-tuple-element.107), channel_id=1, source_target_pairs={{0,16},{8,24},{16,0},{24,8},{1,17},{9,25},{17,1},{25,9},{2,18},{10... | collective-permute-start | bytes 3145736 | tf_op jit(solution)/shard_map/ppermute | solution.py:381
  461.8 23.5 %collective-permute-start.37 = (bf16[256,2048]{1,0:T(8,128)(2,1)S(1)}, bf16[256,2048]{1,0:T(8,128)(2,1)S(1)}, u32[]{:S(2)}, u32[]{:S(2)}) collective-permute-start(bf16[256,2048]{1,0:T(8,128)(2,1)S(1)} %get-tuple-element.107), channel_id=1, source_target_pairs={{0,8},{8,0},{16,24},{24,16},{1,9},{9,1},{17,25},{25,17},{2,10},{10... | collective-permute-start | bytes 3145736 | tf_op jit(solution)/shard_map/ppermute | solution.py:381
  482.3 12.2 %collective-permute-start.39 = (bf16[128,2048]{1,0:T(8,128)(2,1)S(1)}, bf16[128,2048]{1,0:T(8,128)(2,1)S(1)}, u32[]{:S(2)}, u32[]{:S(2)}) collective-permute-start(bf16[128,2048]{1,0:T(8,128)(2,1)S(1)} %slice.286), channel_id=1, source_target_pairs={{0,8},{8,0},{16,24},{24,16},{1,9},{9,1},{17,25},{25,17},{2,10},{10... | collective-permute-start | bytes 1572872 | tf_op jit(solution)/shard_map/ppermute | solution.py:381
  485.4 9.5 %collective-permute-start.40 = (bf16[128,2048]{1,0:T(8,128)(2,1)S(1)}, bf16[128,2048]{1,0:T(8,128)(2,1)S(1)}, u32[]{:S(2)}, u32[]{:S(2)}) collective-permute-start(bf16[128,2048]{1,0:T(8,128)(2,1)S(1)} %slice.287), channel_id=1, source_target_pairs={{0,16},{8,24},{16,0},{24,8},{1,17},{9,25},{17,1},{25,9},{2,18},{10... | collective-permute-start | bytes 1572872 | tf_op jit(solution)/shard_map/ppermute | solution.py:381
  535.3 140.5 %reduce-scatter.11.cloned.1.call-start = ((), (), s32[]{:S(2)}) async-start(), calls=%async_computation.9 | async-start | bytes 2359296 | tf_op jit(solution)/shard_map/reduce_scatter | solution.py:669
  569.3 4.6 collective-permute-start.45
  573.9 4.1 collective-permute-start.46
  578.1 13.8 %collective-permute-start.47 = (f32[4,1352]{1,0:T(4,128)S(1)}, f32[4,1352]{1,0:T(4,128)S(1)}, u32[]{:S(2)}, u32[]{:S(2)}) collective-permute-start(f32[4,1352]{1,0:T(4,128)S(1)} %slice_select_fusion.2), channel_id=1, source_target_pairs={{0,4},{1,5},{2,6},{3,7},{4,0},{5,1},{6,2},{7,3},{8,12},{9,13},{10,... | collective-permute-start | bytes 64904 | tf_op jit(solution)/shard_map/ppermute | solution.py:413
  591.9 4.2 collective-permute-start.48
  593.6 10.0 %collective-permute-start.41 = (bf16[128,2048]{1,0:T(8,128)(2,1)S(1)}, bf16[128,2048]{1,0:T(8,128)(2,1)S(1)}, u32[]{:S(2)}, u32[]{:S(2)}) collective-permute-start(bf16[128,2048]{1,0:T(8,128)(2,1)S(1)} %get-tuple-element.120), channel_id=1, source_target_pairs={{0,16},{8,24},{16,0},{24,8},{1,17},{9,25},{17,1},{25,9},{2,18},{10... | collective-permute-start | bytes 1572872 | tf_op jit(solution)/shard_map/ppermute | solution.py:381
  594.0 10.2 %collective-permute-start.43 = (bf16[128,2048]{1,0:T(8,128)(2,1)S(1)}, bf16[128,2048]{1,0:T(8,128)(2,1)S(1)}, u32[]{:S(2)}, u32[]{:S(2)}) collective-permute-start(bf16[128,2048]{1,0:T(8,128)(2,1)S(1)} %get-tuple-element.119), channel_id=1, source_target_pairs={{0,8},{8,0},{16,24},{24,16},{1,9},{9,1},{17,25},{25,17},{2,10},{10... | collective-permute-start | bytes 1572872 | tf_op jit(solution)/shard_map/ppermute | solution.py:381
  596.1 12.9 %collective-permute-start.49 = (f32[1,1352]{1,0:T(1,128)S(1)}, f32[1,1352]{1,0:T(1,128)S(1)}, u32[]{:S(2)}, u32[]{:S(2)}) collective-permute-start(f32[1,1352]{1,0:T(1,128)S(1)} %broadcast_select_fusion.4), channel_id=1, source_target_pairs={{0,1},{1,0},{2,3},{3,2},{4,5},{5,4},{6,7},{7,6},{8,9},{9,8},{10,11... | collective-permute-start | bytes 16232 | tf_op jit(solution)/shard_map/ppermute | solution.py:413
  605.8 20.3 %collective-permute-start.42 = (bf16[256,2048]{1,0:T(8,128)(2,1)S(1)}, bf16[256,2048]{1,0:T(8,128)(2,1)S(1)}, u32[]{:S(2)}, u32[]{:S(2)}) collective-permute-start(bf16[256,2048]{1,0:T(8,128)(2,1)S(1)} %pad_maximum_fusion.14), channel_id=1, source_target_pairs={{0,8},{8,0},{16,24},{24,16},{1,9},{9,1},{17,25},{25,17},{2,10},{10... | collective-permute-start | bytes 3145736 | tf_op jit(solution)/shard_map/ppermute | solution.py:381
  608.4 19.4 %collective-permute-start.44 = (bf16[256,2048]{1,0:T(8,128)(2,1)}, bf16[256,2048]{1,0:T(8,128)(2,1)S(1)}, u32[]{:S(2)}, u32[]{:S(2)}) collective-permute-start(bf16[256,2048]{1,0:T(8,128)(2,1)} %pad_maximum_fusion.15), channel_id=1, source_target_pairs={{0,16},{8,24},{16,0},{24,8},{1,17},{9,25},{17,1},{25,9},{2,18},{10... | collective-permute-start | bytes 3145736 | tf_op jit(solution)/shard_map/ppermute | solution.py:381
  638.5 8.8 %collective-permute-start.53 = (bf16[64,2816]{1,0:T(8,128)(2,1)S(1)}, bf16[64,2816]{1,0:T(8,128)(2,1)S(1)}, u32[]{:S(2)}, u32[]{:S(2)}) collective-permute-start(bf16[64,2816]{1,0:T(8,128)(2,1)S(1)} %get-tuple-element.158), channel_id=1, source_target_pairs={{0,8},{8,0},{16,24},{24,16},{1,9},{9,1},{17,25},{25,17},{2,10},{10... | collective-permute-start | bytes 1081352 | tf_op jit(solution)/shard_map/ppermute | solution.py:381
  639.6 12.7 %collective-permute-start.54 = (bf16[64,2816]{1,0:T(8,128)(2,1)S(1)}, bf16[64,2816]{1,0:T(8,128)(2,1)S(1)}, u32[]{:S(2)}, u32[]{:S(2)}) collective-permute-start(bf16[64,2816]{1,0:T(8,128)(2,1)S(1)} %get-tuple-element.157), channel_id=1, source_target_pairs={{0,16},{8,24},{16,0},{24,8},{1,17},{9,25},{17,1},{25,9},{2,18},{10... | collective-permute-start | bytes 1081352 | tf_op jit(solution)/shard_map/ppermute | solution.py:381
  641.0 12.8 %collective-permute-start.55 = (bf16[64,2816]{1,0:T(8,128)(2,1)S(1)}, bf16[64,2816]{1,0:T(8,128)(2,1)S(1)}, u32[]{:S(2)}, u32[]{:S(2)}) collective-permute-start(bf16[64,2816]{1,0:T(8,128)(2,1)S(1)} %get-tuple-element.156), channel_id=1, source_target_pairs={{0,24},{8,16},{16,8},{24,0},{1,25},{9,17},{17,9},{25,1},{2,26},{10... | collective-permute-start | bytes 1081352 | tf_op jit(solution)/shard_map/ppermute | solution.py:381
  655.2 6.4 collective-permute-start.50
  656.6 9.2 %collective-permute-start.51 = (bf16[64,2048]{1,0:T(8,128)(2,1)S(1)}, bf16[64,2048]{1,0:T(8,128)(2,1)S(1)}, u32[]{:S(2)}, u32[]{:S(2)}) collective-permute-start(bf16[64,2048]{1,0:T(8,128)(2,1)S(1)} %get-tuple-element.173), channel_id=1, source_target_pairs={{0,16},{8,24},{16,0},{24,8},{1,17},{9,25},{17,1},{25,9},{2,18},{10... | collective-permute-start | bytes 786440 | tf_op jit(solution)/shard_map/ppermute | solution.py:381
  656.6 9.2 %collective-permute-start.52 = (bf16[64,2048]{1,0:T(8,128)(2,1)S(1)}, bf16[64,2048]{1,0:T(8,128)(2,1)S(1)}, u32[]{:S(2)}, u32[]{:S(2)}) collective-permute-start(bf16[64,2048]{1,0:T(8,128)(2,1)S(1)} %get-tuple-element.172), channel_id=1, source_target_pairs={{0,24},{8,16},{16,8},{24,0},{1,25},{9,17},{17,9},{25,1},{2,26},{10... | collective-permute-start | bytes 786440 | tf_op jit(solution)/shard_map/ppermute | solution.py:381
  (76 other events, 690.0 us)
Sparse Core Ops, SparseCore 0:
  32.4 83.6 all-gather.10
  117.6 27.5 all-gather.6
  147.5 107.5 all-gather.12
  256.5 58.7 all-gather.8
  317.4 63.5 reduce-scatter.4
  383.2 117.6 reduce-scatter.6
  535.4 94.3 reduce-scatter.8
  633.2 35.3 reduce-scatter.10

commit v3 on v2

--- a/solution.py
+++ b/solution.py
@@ -373,6 +373,214 @@
     )
 
 
+def peers(ring, mine):
+    found = []
+    for by in range(1, ring):
+        at, bit = mine, 1
+        while bit <= by:
+            if by & bit:
+                at = at + bit * (1 - 2 * ((at // bit) % 2))
+            bit *= 2
+        found.append(at)
+    return found
+
+
+class Copies:
+    def __init__(self, local, send, recv):
+        self.local, self.send, self.recv = local, send, recv
+        self.here, self.away = 0, 0
+        self.open = []
+
+    def near(self, source, target):
+        copy = pltpu.make_async_copy(source, target, self.local.at[self.here])
+        self.here += 1
+        copy.start()
+        return copy
+
+    def far(self, source, target, landed, device, when=None):
+        at = self.away
+        self.away += 1
+        copy = pltpu.make_async_remote_copy(
+            source, target, self.send.at[at], self.recv.at[at], device_id=device,
+            device_id_type=pl.DeviceIdType.MESH,
+        )
+        if when is None:
+            copy.start()
+        else:
+            pl.when(when)(copy.start)
+        self.open.append((copy, when))
+        return pltpu.make_async_remote_copy(
+            landed, landed, self.send.at[at], self.recv.at[at], device_id=device,
+            device_id_type=pl.DeviceIdType.MESH,
+        ).wait_recv
+
+    def close(self):
+        for copy, when in self.open:
+            if when is None:
+                copy.wait_send()
+            else:
+                pl.when(when)(copy.wait_send)
+
+
+def slab_chain(copies, chips, place):
+    mine, batch = lax.axis_index("seq"), lax.axis_index("batch")
+    chip, core = batch // 2, batch % 2
+    other = (mine, chip * 2 + (1 - core))
+
+    def at(where):
+        return jnp.clip(where, 0, chips - 1) * 2 + core
+
+    def send(step, way):
+        block, come = chip - way * (step - 1), chip - way * step
+        when = (block >= 0) & (block < chips) & (chip + way >= 0) & (chip + way < chips)
+        came = (come >= 0) & (come < chips)
+        wait = copies.far(
+            place(at(block)), place(at(block)), place(at(come)), (mine, at(chip + way)), when
+        )
+        return wait, came, at(come)
+
+    crossing = [(copies.far(place(batch), place(batch), place(other[1]), other), None)]
+    flying = [send(1, 1), send(1, -1)] if chips > 1 else []
+    yield
+    for step in range(1, chips):
+        coming = []
+        for way, (wait, came, landed) in zip((1, -1), flying):
+            pl.when(came)(wait)
+            if step + 1 < chips:
+                coming.append(send(step + 1, way))
+            there = landed + 1 - 2 * core
+            crossing.append(
+                (copies.far(place(landed), place(landed), place(there), other, came), came)
+            )
+        flying = coming
+        yield
+    for wait, came in crossing:
+        if came is None:
+            wait()
+        else:
+            pl.when(came)(wait)
+    yield
+
+
+def start_kernel(
+    ring, lines, inputs, w_query, w_key, w_value, w_swish, w_out, gate, up, small,
+    inputs_all, w_mixer, w_output, feed_columns, small_all, local_sem, send_sem, recv_sem,
+):
+    mine, batch = lax.axis_index("seq"), lax.axis_index("batch")
+    chips = lines // 2
+    copies = Copies(local_sem, send_sem, recv_sem)
+    part = w_mixer.shape[3] // 4
+    half = inputs.shape[0] // 2
+    others = peers(ring, mine)
+    pieces = (w_query, w_key, w_value, w_swish)
+
+    def column(ref, at):
+        if len(ref.shape) == 3:
+            return ref.at[at]
+        size = ref.shape[1] // ring
+        return ref.at[:, pl.ds(pl.multiple_of(at * size, 128), size)]
+
+    def slot(source, piece):
+        return w_mixer.at[source, batch, :, pl.ds(piece * part, part)]
+
+    near = [copies.near(column(ref, mine), slot(mine, at)) for at, ref in enumerate(pieces)]
+    near += [copies.near(w_out, w_output.at[batch]), copies.near(small, small_all.at[mine, batch])]
+    column_waits, small_waits = [], []
+    for to in others:
+        column_waits.append(
+            [
+                copies.far(column(ref, to), slot(mine, at), slot(to, at), (to, batch))
+                for at, ref in enumerate(pieces)
+            ]
+        )
+        small_waits.append(
+            copies.far(small, small_all.at[mine, batch], small_all.at[to, batch], (to, batch))
+        )
+    own_input = copies.near(inputs, inputs_all.at[0])
+    direct = 2 if ring == 4 else ring - 1
+    input_waits = [
+        copies.far(inputs, inputs_all.at[by + 1], inputs_all.at[by + 1], (others[by], batch))
+        for by in range(direct)
+    ]
+    for copy in near:
+        copy.wait()
+
+    def started(place):
+        chain = slab_chain(copies, chips, place)
+        next(chain)
+        chains.append(chain)
+
+    chains = []
+    started(lambda at: w_mixer.at[mine, at])
+    for waits, source in zip(column_waits, others):
+        for wait in waits:
+            wait()
+        started(lambda at, source=source: w_mixer.at[source, at])
+    for wait, source in zip(small_waits, others):
+        wait()
+        started(lambda at, source=source: small_all.at[source, at])
+    started(lambda at: small_all.at[mine, at])
+    started(lambda at: w_output.at[at])
+    own_feed = [copies.near(column(ref, mine), feed_columns.at[at, mine]) for at, ref in enumerate((gate, up))]
+    for chain in chains:
+        if chips > 1:
+            next(chain)
+    if ring == 4:
+        for wait in input_waits:
+            wait()
+        low, high = pl.ds(0, half), pl.ds(half, half)
+        input_waits = [
+            copies.far(
+                inputs_all.at[have, rows], inputs_all.at[3, rows], inputs_all.at[3, rows], (to, batch)
+            )
+            for have, rows, to in ((2, low, others[0]), (1, high, others[1]))
+        ]
+    feed_waits = [
+        copies.far(
+            column(ref, to), feed_columns.at[at, mine], feed_columns.at[at, to], (to, batch)
+        )
+        for to in others
+        for at, ref in enumerate((gate, up))
+    ]
+    for _ in range(chips - 1 if chips > 1 else 1):
+        for chain in chains:
+            next(chain)
+    for wait in input_waits + feed_waits:
+        wait()
+    for copy in [own_input] + own_feed:
+        copy.wait()
+    copies.close()
+
+
+def start(ring, lines, inputs, columns, w_out, gate, up, small):
+    own, width = columns[0].shape
+    part, hidden = width // ring, gate.shape[1] // ring
+    if hidden % 128:
+        gate, up = (a.reshape(own, ring, hidden).transpose(1, 0, 2) for a in (gate, up))
+    chains = 2 * ring + 1
+    away = (ring - 1) * 8 + 4 + chains * (4 * (lines // 2 - 1) + 1)
+    anywhere = pl.BlockSpec(memory_space=pl.ANY)
+    return pl.pallas_call(
+        functools.partial(start_kernel, ring, lines),
+        out_shape=(
+            jax.ShapeDtypeStruct((ring,) + inputs.shape, BF16),
+            jax.ShapeDtypeStruct((ring, lines, own, 4 * part), BF16),
+            jax.ShapeDtypeStruct((lines,) + w_out.shape, BF16),
+            jax.ShapeDtypeStruct((2, ring, own, hidden), BF16),
+            jax.ShapeDtypeStruct((ring, lines) + small.shape, BF16),
+        ),
+        in_specs=[anywhere] * 9,
+        out_specs=[anywhere] * 5,
+        scratch_shapes=[
+            pltpu.SemaphoreType.DMA((12,)),
+            pltpu.SemaphoreType.DMA((away,)),
+            pltpu.SemaphoreType.DMA((away,)),
+        ],
+        compiler_params=pltpu.CompilerParams(has_side_effects=True),
+        name="start",
+    )(inputs, *columns, w_out, gate, up, small)
+
+
 def rms_scale(features):
     return lax.rsqrt(jnp.mean(features * features, axis=-1, keepdims=True) + EPS)
 
@@ -484,16 +692,6 @@
     hidden_part = gate_weight.shape[1] // ring
     slots_all = HEADS * SLOTS
 
-    def permuted(array):
-        shape = array.shape[:-1]
-        array = array.reshape(shape + (ring, lines, own))
-        return jnp.swapaxes(array, -3, -2).reshape(shape + (width,))
-
-    def restored(array):
-        shape = array.shape[:-1]
-        array = array.reshape(shape + (lines, ring, own))
-        return jnp.swapaxes(array, -3, -2).reshape(shape + (width,))
-
     def to_order(array):
         if copies == 1:
             return array
@@ -512,7 +710,7 @@
             return array
         return lax.dynamic_slice_in_dim(array, (mine % copies) * part, part, 1)
 
-    small = jnp.concatenate(
+    params = jnp.concatenate(
         [
             mixer_gain,
             head_gain,
@@ -522,10 +720,32 @@
             squeeze.reshape(-1),
         ]
     )
-    small = doubled(doubled(small[None], "batch"), "seq")
+    count = params.shape[0]
+    params = jnp.concatenate([params, segments.reshape(rows).astype(BF16)])
+    params = jnp.pad(params, (0, -params.shape[0] % 2048)).reshape(-1, 128)
+    input_own = layer_input.reshape(rows, width)
+    inputs, w_mixer, w_output, feed_columns, small = start(
+        ring,
+        lines,
+        input_own,
+        (query_weight, key_weight, value_weight, swish_weight),
+        output_weight,
+        gate_weight,
+        up_weight,
+        params,
+    )
+    inputs = inputs.reshape(length, width)
+    w_mixer = w_mixer.reshape(width, 4 * part)
+    w_output = w_output.reshape(part, width)
+    small = small.reshape(devices, -1)
+    segment = lax.dynamic_index_in_dim(
+        small.reshape(ring, lines, -1), lax.axis_index("batch"), 1, keepdims=False
+    )[:, count : count + rows].reshape(length).astype(F32)
     cuts = np.cumsum([own, own, own, slots_all // devices, RANK * slots_all // devices])
-    gain_one, gain_head, gain_two, bias_full, expand_t, w_squeeze = jnp.split(small, cuts, axis=1)
-    gain_one = permuted(gain_one.reshape(width)).astype(F32)
+    gain_one, gain_head, gain_two, bias_full, expand_t, w_squeeze = jnp.split(
+        small[:, :count], cuts, axis=1
+    )
+    gain_one = gain_one.reshape(width).astype(F32)
     gain_head = lax.dynamic_slice_in_dim(gain_head.reshape(width), head * head_size, head_size, 0)
     gain_head = gain_head.astype(F32)
     gain_two = gain_two.reshape(width).astype(F32)
@@ -533,24 +753,16 @@
     expand_head = lax.dynamic_slice_in_dim(
         expand_t.reshape(slots_all, RANK), head * SLOTS, SLOTS, 0
     )
-    w_squeeze = permuted(w_squeeze.reshape(width, RANK).T)
-
-    def columns(*arrays):
-        blocks = [a.reshape(own, ring, a.shape[1] // ring) for a in arrays]
-        return jnp.concatenate(blocks, axis=2).transpose(1, 0, 2)
-
-    mixer_columns = exchanged(
-        columns(query_weight, key_weight, value_weight, swish_weight), mine, ring
-    )
-    w_mixer = lax.all_gather(mixer_columns, "batch", axis=0, tiled=False).reshape(width, 4 * part)
-    w_output = lax.all_gather(output_weight, "batch", axis=0, tiled=True)
-    feed_columns = exchanged(columns(gate_weight, up_weight), mine, ring)
-    w_feed = lax.all_gather(feed_columns, "batch", axis=0, tiled=False).reshape(
-        width, 2 * hidden_part
-    )
-    w_down = lax.all_gather(down_weight, "batch", axis=0, tiled=True)
-
-    segment = doubled(segments.reshape(1, rows), "seq").reshape(length).astype(F32)
+    w_squeeze = w_squeeze.reshape(width, RANK).T
+
+    feed_blocks = lax.all_gather(
+        feed_columns.reshape(2 * ring * own, hidden_part), "batch", axis=0, tiled=False
+    )
+    feed_blocks = feed_blocks.reshape(lines, 2, ring, own, hidden_part)
+    feed_blocks = feed_blocks.transpose(1, 2, 0, 3, 4).reshape(2, width, hidden_part)
+    w_gate, w_up = feed_blocks[0], feed_blocks[1]
+    w_down = lax.all_gather(after(down_weight, inputs), "batch", axis=0, tiled=True)
+
     chunked = segment.reshape(-1, CHUNK)
     before = jnp.concatenate([jnp.full((1,), -1.0, F32), chunked[:-1, -1]])
     previous = jnp.concatenate([jnp.full((1,), -1.0, F32), segment[:-1]])
@@ -565,8 +777,6 @@
     )
     segment_col = segment[:, None]
 
-    input_own = layer_input.reshape(rows, width)
-    inputs = gathered(permuted(input_own), ring)
     grad_own = cotangent.reshape(rows, width)
     grad_out = gathered(after(grad_own, inputs), ring)
     inputs = inputs.astype(F32)
@@ -583,6 +793,7 @@
     log_rate = jax.nn.log_sigmoid(forget_logit) / TAU_GATE
     inflow = -jnp.expm1(log_rate)
     order = mine.reshape(1).astype(jnp.int32)
+    query, grad_out = lax.optimization_barrier((query, grad_out))
     mixed, attention, logits, key_start, value_start = mixer_forward(
         order, ring, query, key, value, log_rate, inflow, mask_rows, segment_col
     )
@@ -595,9 +806,8 @@
     hidden = input_own.astype(F32) + scattered(dot_nn(gated, w_output).astype(BF16), ring)
 
     scale_two = rms_scale(hidden)
-    feed_in = gathered(permuted((hidden * scale_two * gain_two).astype(BF16)), ring)
-    feed_pre = dot_nn(feed_in, w_feed)
-    gate_pre, up_pre = feed_pre[:, :hidden_part], feed_pre[:, hidden_part:]
+    feed_in = gathered(((hidden * scale_two * gain_two).astype(BF16)), ring)
+    gate_pre, up_pre = dot_nn(feed_in, w_gate), dot_nn(feed_in, w_up)
     gate_sig = jax.nn.sigmoid(gate_pre)
     gate_act = gate_pre * gate_sig
     inner = (gate_act * up_pre).astype(BF16)
@@ -605,20 +815,25 @@
     term_down = dot_tn(inner, grad_out).astype(BF16)
     grad_inner = dot_nt(after(grad_out, term_down), w_down)
     grad_gatepre = grad_inner * up_pre * (gate_sig * (1.0 + gate_pre * (1.0 - gate_sig)))
-    grad_feedpre = jnp.concatenate(
-        [grad_gatepre.astype(BF16), (grad_inner * gate_act).astype(BF16)], axis=1
-    )
-    back_feedin = dot_nt(grad_feedpre, w_feed).astype(BF16)
-    grad_feedin = restored(scattered(back_feedin, ring))
-    term_feedpre = dot_tn(feed_in, after(grad_feedpre, back_feedin)).astype(BF16)
-    result = hidden + scattered(dot_nn(after(inner, term_feedpre), w_down).astype(BF16), ring)
+    grad_gatepre = grad_gatepre.astype(BF16)
+    grad_uppre = (grad_inner * gate_act).astype(BF16)
+    back_feedin = (dot_nt(grad_gatepre, w_gate) + dot_nt(grad_uppre, w_up)).astype(BF16)
+    grad_feedin = scattered(back_feedin, ring)
+    feed_rows = after(feed_in, back_feedin)
+    term_gate = dot_tn(feed_rows, grad_gatepre).astype(BF16)
+    term_up = dot_tn(feed_rows, grad_uppre).astype(BF16)
+    result = hidden + scattered(dot_nn(after(inner, term_gate, term_up), w_down).astype(BF16), ring)
     layer_output = result.astype(BF16).reshape(1, rows, width)
     down_share = lax.psum_scatter(term_down, "batch", scatter_dimension=0, tiled=True)
-    feed_share = lax.psum_scatter(after(term_feedpre, down_share), "batch", scatter_dimension=0, tiled=True)
-    feed_sum = feed_share
-    feed_share = exchanged(feed_share.reshape(ring, own, 2 * hidden_part), mine, ring)
-    gate_share = feed_share[:, :, :hidden_part].transpose(1, 0, 2).reshape(own, -1)
-    up_share = feed_share[:, :, hidden_part:].transpose(1, 0, 2).reshape(own, -1)
+    term_feedpre = jnp.stack([term_gate, term_up]).reshape(2, ring, lines, own, hidden_part)
+    term_feedpre = term_feedpre.transpose(2, 0, 1, 3, 4).reshape(-1, hidden_part)
+    feed_sum = lax.psum_scatter(
+        after(term_feedpre, down_share), "batch", scatter_dimension=0, tiled=True
+    )
+    feed_share = feed_sum.reshape(2, ring, own, hidden_part).transpose(1, 0, 2, 3)
+    feed_share = exchanged(feed_share, mine, ring)
+    gate_share = feed_share[:, 0].transpose(1, 0, 2).reshape(own, -1)
+    up_share = feed_share[:, 1].transpose(1, 0, 2).reshape(own, -1)
     term_feed = jnp.sum(grad_feedin * hidden * scale_two, axis=0)
     scaled_two = grad_feedin * gain_two
     grad_hidden = (
@@ -627,7 +842,7 @@
         - hidden * scale_two**3 * jnp.mean(scaled_two * hidden, axis=-1, keepdims=True)
     )
 
-    grad_branch = after(gathered(grad_hidden.astype(BF16), ring), term_feedpre)
+    grad_branch = after(gathered(grad_hidden.astype(BF16), ring), term_gate, term_up)
     grad_gated = whole_head(dot_nt(grad_branch, w_output))
     term_output = dot_tn(gated, grad_branch).astype(BF16)
     slope = swish_sig * (1.0 + swish_pre * (1.0 - swish_sig))
@@ -661,10 +876,12 @@
         [own_part(grad_query), own_part(grad_key), own_part(grad_value), grad_swishpre], axis=1
     )
     grad_normed = dot_nt(grad_pre, w_mixer) + dot_nn(grad_reduced, w_squeeze)
-    term_mixer = restored(jnp.sum(grad_normed * plain_one, axis=0))
-    term_squeeze = restored(dot_tn(grad_reduced, normed))
+    term_mixer = (jnp.sum(grad_normed * plain_one, axis=0))
+    term_squeeze = (dot_tn(grad_reduced, normed))
     term_pre = dot_tn(normed, grad_pre).astype(BF16)
-    grad_normed = restored(scattered(after(grad_normed.astype(BF16), term_pre), ring))
+    term_pre = term_pre.reshape(ring, lines, own, 4 * part).transpose(1, 0, 2, 3)
+    term_pre = term_pre.reshape(width, 4 * part)
+    grad_normed = (scattered(after(grad_normed.astype(BF16), term_pre), ring))
     pre_share = lax.psum_scatter(after(term_pre, feed_sum), "batch", scatter_dimension=0, tiled=True)
     output_share = lax.psum_scatter(
         after(term_output, pre_share), "batch", scatter_dimension=0, tiled=True
@@ -674,7 +891,7 @@
     pre_share = pre_share.astype(F32)
     inputs_own = input_own.astype(F32)
     scale_own = rms_scale(inputs_own)
-    scaled_one = grad_normed * restored(gain_one)
+    scaled_one = grad_normed * (gain_one)
     grad_inputs = (
         grad_hidden
         + scale_own * scaled_one

time: 694 us -> 711 us (1.024)
  Pallas kernels: 31.6 us -> 149 us
  waiting for transfers between devices: 256 us -> 199 us
  local copies, waits for them, and re-layouts: 114 us -> 90.4 us
  starting transfers between devices: 65.4 us -> 50.9 us
    pallas_call x0 -> x1, Pallas kernels: none -> 117 us  [start(): pl.pallas_call(functools.partial(start_kernel, ring, lines), out_shape=(j...]
    ppermute x12 -> x5, waiting for transfers between devices: 41.9 us -> 7.72 us  [flipped(): lax.ppermute(block, axis, [(i, i ^ by) for i in range(lax.axis_size(axis))])]
    ppermute x44 -> x34, waiting for transfers between devices: 194 us -> 163 us  [swapped(): return lax.ppermute(block, 'seq', [(i, i ^ by) for i in range(ring)])]
    reduce_scatter x1, waiting for transfers between devices: 0.02 us -> 22 us  [local(): lax.psum_scatter(after(term_pre, feed_sum), 'batch', scatter_dimension=0,...]
    slice x0 -> x6, local copies, waits for them, and re-layouts: none -> 14.7 us  [the longest x3 13.7 us: local(): w_gate, w_up = (feed_blocks[0], feed_blocks[1])]
    unnamed x191 -> x184, local copies, waits for them, and re-layouts: 41.9 us -> 30.2 us
    convert_element_type x5 -> x2, local copies, waits for them, and re-layouts: 10.5 us -> 0.08 us  [the longest x1 0.07 us: local(): gain_one = gain_one.reshape(width).astype(F32)]
    ppermute x44 -> x34, starting transfers between devices: 49 us -> 39 us  [swapped(): return lax.ppermute(block, 'seq', [(i, i ^ by) for i in range(ring)])]
  transfers between devices with their start and end apart: 64 -> 45, of which waited for: 41 -> 30; matrix products, arithmetic and copies ran while one was open for 42% -> 39% of each run, Pallas kernels for 5% -> 5%
where the time goes in v3:
time: 711 us; the launch traced here: 706 us
  waiting for transfers between devices  199 us (28%)
  matrix products  153 us (22%)
  Pallas kernels  149 us (21%)
  local copies, waits for them, and re-layouts  90.4 us (13%)
  starting transfers between devices  50.9 us (7%)
  other arithmetic  47.8 us (7%)
  between operations  15.8 us (2%)
    ppermute x34, waiting for transfers between devices, swapped(): return lax.ppermute(block, 'seq', [(i, i ^ by) for i in range(ring)])  163 us
    pallas_call x1, Pallas kernels, start(): pl.pallas_call(functools.partial(start_kernel, ring, lines), out_shape=(j...  117 us
    dot_general x7, matrix products, dot_nt(): lax.dot_general(left, right, (((1,), (1,)), ((), ())), preferred_element_...  55.2 us
    dot_general x7, matrix products, dot_nn(): lax.dot_general(left, right, (((1,), (0,)), ((), ())), preferred_element_...  52.8 us
    dot_general x7, matrix products, dot_tn(): lax.dot_general(left, right, (((0,), (0,)), ((), ())), preferred_element_...  45.3 us
    ppermute x34, starting transfers between devices, swapped(): return lax.ppermute(block, 'seq', [(i, i ^ by) for i in range(ring)])  39 us
    unnamed x184, local copies, waits for them, and re-layouts  30.2 us
    reduce_scatter x1, waiting for transfers between devices, local(): lax.psum_scatter(after(term_pre, feed_sum), 'batch', scatter_dimension=0,...  22 us
  transfers between devices with their start and end apart: 45, of which 30 were waited for; matrix products, arithmetic and copies ran while one was open for 39% of the time, Pallas kernels for 5%

profile of v3, /device:TPU:0, one launch (start us, length us, event | category | flops | bytes accessed | tf_op | source)
XLA Modules:
  0.0 706.0 jit_solution(8359727759536331187)
XLA Ops:
  9.6 2.8 concatenate.67
  12.9 116.9 %start.1 = (bf16[4,256,2048]{2,1,0:T(8,128)(2,1)}, bf16[4,8,64,2048]{3,2,1,0:T(8,128)(2,1)}, bf16[8,64,2048]{2,1,0:T(8,128)(2,1)}, bf16[2,4,64,1408]{3,2,1,0:T(8,128)(2,1)}, bf16[4,8,16,128]{3,2,1,0:T(8,128)(2,1)}) custom-call(bf16[256,2048]{1,0:T(8,128)(2,1)} %bitcast.177, bf16[64,2048]{1,0:T(8,128)(2,1)} %w_query.1, bf16[64,2048]{1,0:T(8,128)(2,1)} %w_key.1, ...), custom_call_target="tpu_custom_call" | custom-call | tf_op jit(solution)/shard_map/start/pallas_call | solution.py:563
  136.2 4.1 fusion
  143.7 12.1 %fusion.34 = (bf16[1024,2048]{1,0:T(8,128)(2,1)}, f32[1024,2048]{1,0:T(8,128)}) fusion(bf16[1024,2048]{1,0:T(8,128)(2,1)S(1)} %bitcast.176, bf16[2048,2048]{1,0:T(8,128)(2,1)S(1)} %bitcast.229), kind=kOutput, calls=%fused_computation.180 | convolution fusion | flops 8592031744 | bytes 25165824 | tf_op jit(solution)/shard_map/dot_general | solution.py:25
  158.4 2.3 constant_dynamic-update-slice_fusion.4
  160.7 2.1 fusion.32
  168.5 2.3 constant_dynamic-update-slice_fusion.3
  170.8 2.4 constant_dynamic-update-slice_fusion.2
  173.2 5.8 collective-permute-done.2
  182.7 11.1 %mixer_forward.1 = (f32[1024,512]{1,0:T(8,128)S(1)}, f32[64,1024]{1,0:T(8,128)S(1)}, f32[64,1024]{1,0:T(8,128)S(1)}, f32[8,64,512]{2,1,0:T(8,128)S(1)}, f32[8,64,512]{2,1,0:T(8,128)S(1)}) custom-call(s32[1]{0:T(128)} %bitcast.1.mine, bf16[1024,512]{1,0:T(8,128)(2,1)S(1)} %get-tuple-element.46.query, bf16[1024,512]{1,0:T(8,128)(2,1)S(1)} %get-tuple-element.164.key, ...), custom_call_target="tpu_custom_call" | custom-call | flops 1048576000 | bytes 6291456 | tf_op jit(solution)/shard_map/mixer_forward/pallas_call | solution.py:311
  194.7 3.7 multiply_convert_fusion.6
  199.4 2.3 convolution_convert_fusion.5
  204.1 10.6 %collective-permute-done.4 = bf16[128,2048]{1,0:T(8,128)(2,1)S(1)} collective-permute-done((bf16[128,2048]{1,0:T(8,128)(2,1)S(1)}, bf16[128,2048]{1,0:T(8,128)(2,1)S(1)}, u32[]{:S(2)}, u32[]{:S(2)}) %collective-permute-start.4) | collective-permute-done | bytes 524320 | tf_op jit(solution)/shard_map/ppermute | solution.py:589
  220.9 19.0 %collective-permute-done.7 = bf16[256,2048]{1,0:T(8,128)(2,1)} collective-permute-done((bf16[256,2048]{1,0:T(8,128)(2,1)}, bf16[256,2048]{1,0:T(8,128)(2,1)}, u32[]{:S(2)}, u32[]{:S(2)}) %collective-permute-start.7) | collective-permute-done | bytes 1048608 | tf_op jit(solution)/shard_map/ppermute | solution.py:589
  239.9 2.2 collective-permute-done.5
  242.1 2.9 multiply_reduce_fusion.5
  250.9 19.1 %collective-permute-done.9 = bf16[256,2048]{1,0:T(8,128)(2,1)} collective-permute-done((bf16[256,2048]{1,0:T(8,128)(2,1)}, bf16[256,2048]{1,0:T(8,128)(2,1)}, u32[]{:S(2)}, u32[]{:S(2)}) %collective-permute-start.9) | collective-permute-done | bytes 1048608 | tf_op jit(solution)/shard_map/ppermute | solution.py:589
  271.1 2.0 collective-permute-start.10
  275.2 2.3 constant_dynamic-update-slice_fusion.7
  277.5 4.7 collective-permute-done.10
  284.0 9.9 %fusion.27 = (bf16[1,4,8,64,1408]{4,3,1,0,2:T(8,128)(2,1)}, bf16[1,4,8,64,1408]{4,3,1,0,2:T(8,128)(2,1)}) fusion(bf16[2,4,8,64,1408]{4,3,1,0,2:T(8,128)(2,1)} %bitcast.178), kind=kLoop, calls=%fused_computation.173 | loop fusion | bytes 23068672 | tf_op jit(solution)/shard_map/slice | solution.py:763
  293.8 3.3 copy.78
  299.6 11.6 %fusion.35 = f32[1024,1408]{1,0:T(8,128)} fusion(bf16[1024,2048]{1,0:T(8,128)(2,1)} %constant_dynamic-update-slice_fusion.5, bf16[2048,1408]{1,0:T(8,128)(2,1)S(1)} %bitcast.181), kind=kOutput, calls=%fused_computation.181 | convolution fusion | flops 5905580032 | bytes 15728640 | tf_op jit(solution)/shard_map/dot_general | solution.py:25
  311.3 10.6 %multiply_convert_fusion.3 = (bf16[1024,1408]{1,0:T(8,128)(2,1)S(1)}, f32[1024,1408]{1,0:T(8,128)}) fusion(f32[1024,1408]{1,0:T(8,128)} %fusion.35, bf16[1024,2048]{1,0:T(8,128)(2,1)S(1)} %copy-done.50, bf16[2048,1408]{1,0:T(8,128)(2,1)S(1)} %bitcast.183), kind=kOutput, calls=%fused_computation.16 | convolution fusion | flops 5914230784 | bytes 24379392 | tf_op jit(solution)/shard_map/dot_general | solution.py:25
  323.4 8.1 %convolution_convert_fusion.3 = bf16[1408,2048]{1,0:T(8,128)(2,1)} fusion(bf16[1024,1408]{1,0:T(8,128)(2,1)S(1)} %get-tuple-element.54, bf16[1024,2048]{1,0:T(8,128)(2,1)S(1)} %copy-done.52), kind=kOutput, calls=%fused_computation.13 | convolution fusion | flops 5908463616 | bytes 12845056 | tf_op jit(solution)/shard_map/dot_general | solution.py:33
  331.8 15.8 %multiply_convert_fusion.1 = (bf16[1024,1408]{1,0:T(8,128)(2,1)}, bf16[1024,1408]{1,0:T(8,128)(2,1)S(1)}) fusion(f32[1024,1408]{1,0:T(8,128)} %fusion.35, f32[1024,1408]{1,0:T(8,128)} %get-tuple-element.215, bf16[1024,2048]{1,0:T(8,128)(2,1)} %constant_dynamic-update-slice_fusion, bf16[1408,2048]{1,0:T(8,128)(2,1)} %all-gather.5.cloned.1.call-done), kind=kOutput, calls=%fused_computation.14 | convolution fusion | flops 5924323328 | bytes 27262976 | tf_op jit(solution)/shard_map/dot_general | solution.py:29
  347.7 8.7 %fusion.36 = f32[1024,2048]{1,0:T(8,128)S(1)} fusion(bf16[1024,1408]{1,0:T(8,128)(2,1)S(1)} %get-tuple-element.134, bf16[2048,1408]{1,0:T(8,128)(2,1)} %bitcast.182), kind=kOutput, calls=%fused_computation.182 | convolution fusion | flops 5905580032 | bytes 17039360 | tf_op jit(solution)/shard_map/dot_general | solution.py:29
  356.4 11.2 %add_convert_fusion = bf16[1024,2048]{1,0:T(8,128)(2,1)} fusion(f32[1024,2048]{1,0:T(8,128)S(1)} %fusion.36, bf16[1024,1408]{1,0:T(8,128)(2,1)} %get-tuple-element.133, bf16[2048,1408]{1,0:T(8,128)(2,1)} %bitcast.184), kind=kOutput, calls=%fused_computation.9 | convolution fusion | flops 5909774336 | bytes 21233664 | tf_op jit(solution)/shard_map/dot_general | solution.py:29
  367.6 7.1 convolution_convert_fusion.2
  374.7 7.1 %convolution_convert_fusion.1 = bf16[2048,1408]{1,0:T(8,128)(2,1)S(1)} fusion(bf16[1024,2048]{1,0:T(8,128)(2,1)S(1)} %copy-done.51, bf16[1024,1408]{1,0:T(8,128)(2,1)S(1)} %copy-done.76), kind=kOutput, calls=%fused_computation.11 | convolution fusion | flops 5908463616 | bytes 12845056 | tf_op jit(solution)/shard_map/dot_general | solution.py:33
  383.7 5.5 copy.97
  389.2 6.5 reduce-scatter.5.cloned.1.call-done
  400.6 9.8 %convolution_convert_fusion.4 = bf16[1024,2048]{1,0:T(8,128)(2,1)S(1)} fusion(bf16[1024,1408]{1,0:T(8,128)(2,1)S(1)} %copy-done.75, bf16[1408,2048]{1,0:T(8,128)(2,1)} %all-gather.5.cloned.1.call-done), kind=kOutput, calls=%fused_computation.21 | convolution fusion | flops 5907677184 | bytes 12845056 | tf_op jit(solution)/shard_map/dot_general | solution.py:25
  413.5 2.1 collective-permute-start.17
  415.6 10.0 %collective-permute-done.12 = bf16[128,2048]{1,0:T(8,128)(2,1)S(1)} collective-permute-done((bf16[128,2048]{1,0:T(8,128)(2,1)S(1)}, bf16[128,2048]{1,0:T(8,128)(2,1)S(1)}, u32[]{:S(2)}, u32[]{:S(2)}) %collective-permute-start.12) | collective-permute-done | bytes 524320 | tf_op jit(solution)/shard_map/ppermute | solution.py:589
  426.1 2.0 collective-permute-start.15
  428.3 19.7 %collective-permute-done.19 = bf16[256,2048]{1,0:T(8,128)(2,1)S(1)} collective-permute-done((bf16[256,2048]{1,0:T(8,128)(2,1)S(1)}, bf16[256,2048]{1,0:T(8,128)(2,1)S(1)}, u32[]{:S(2)}, u32[]{:S(2)}) %collective-permute-start.19) | collective-permute-done | bytes 1048608 | tf_op jit(solution)/shard_map/ppermute | solution.py:589
  448.1 17.7 %collective-permute-done.15 = bf16[256,2048]{1,0:T(8,128)(2,1)S(1)} collective-permute-done((bf16[256,2048]{1,0:T(8,128)(2,1)S(1)}, bf16[256,2048]{1,0:T(8,128)(2,1)S(1)}, u32[]{:S(2)}, u32[]{:S(2)}) %collective-permute-start.15) | collective-permute-done | bytes 1048608 | tf_op jit(solution)/shard_map/ppermute | solution.py:589
  466.6 2.5 multiply_reduce_fusion.1
  469.1 3.7 constant_dynamic-update-slice_fusion.14
  474.9 19.3 %collective-permute-done.21 = bf16[256,2048]{1,0:T(8,128)(2,1)S(1)} collective-permute-done((bf16[256,2048]{1,0:T(8,128)(2,1)S(1)}, bf16[256,2048]{1,0:T(8,128)(2,1)S(1)}, u32[]{:S(2)}, u32[]{:S(2)}) %collective-permute-start.21) | collective-permute-done | bytes 1048608 | tf_op jit(solution)/shard_map/ppermute | solution.py:589
  494.2 3.1 collective-permute-start.22
  498.9 7.7 %collective-permute-done.22 = bf16[128,2048]{1,0:T(8,128)(2,1)S(1)} collective-permute-done((bf16[128,2048]{1,0:T(8,128)(2,1)S(1)}, bf16[128,2048]{1,0:T(8,128)(2,1)S(1)}, u32[]{:S(2)}, u32[]{:S(2)}) %collective-permute-start.22) | collective-permute-done | bytes 524320 | tf_op jit(solution)/shard_map/ppermute | solution.py:589
  507.3 3.2 multiply_reduce_fusion.2
  512.7 20.8 %mixer_backward.1 = (bf16[1024,512]{1,0:T(8,128)(2,1)S(1)}, bf16[1024,512]{1,0:T(8,128)(2,1)S(1)}, bf16[1024,512]{1,0:T(8,128)(2,1)S(1)}, f32[64,1024]{1,0:T(8,128)S(1)}) custom-call(s32[1]{0:T(128)} %bitcast.1.mine, bf16[1024,512]{1,0:T(8,128)(2,1)S(1)} %get-tuple-element.46.query, bf16[1024,512]{1,0:T(8,128)(2,1)S(1)} %get-tuple-element.164.key, ...), custom_call_target="tpu_custom_call" | custom-call | flops 2097152000 | bytes 10485760 | tf_op jit(solution)/shard_map/mixer_backward/pallas_call | solution.py:346
  534.2 12.4 %convolution_convert_fusion = bf16[2048,2048]{1,0:T(8,128)(2,1)} fusion(bf16[1024,2048]{1,0:T(8,128)(2,1)S(1)} %bitcast.173, f32[2048]{0:T(1024)S(1)} %copy-done.57, f32[1024]{0:T(1024)S(1)} %bitcast.216, bf16[1024,512]{1,0:T(8,128)(2,1)S(1)} %get-tuple-element.132, bf16[1024,512]{1,0:T(8,128)(2,1)S(1)} %get-tuple-element.62, ...), kind=kOutput, calls=%fused_computation.10 | convolution fusion | flops 8619294720 | bytes 16789504 | tf_op jit(solution)/shard_map/dot_general | solution.py:33
  546.6 8.4 %copy.83 = bf16[4,8,64,2048]{3,2,0,1:T(8,128)(2,1)} copy(bf16[4,8,64,2048]{3,2,1,0:T(8,128)(2,1)} %bitcast.179) | data formatting | bytes 16777216 | tf_op jit(solution)/shard_map/reshape | solution.py:882
  558.6 13.8 %fusion.14 = f32[1024,2048]{1,0:T(8,128)} fusion(bf16[2048,2048]{1,0:T(8,128)(2,1)} %bitcast.226, bf16[1024,512]{1,0:T(8,128)(2,1)} %copy-done.45, bf16[1024,512]{1,0:T(8,128)(2,1)S(1)} %copy-done.29, bf16[1024,512]{1,0:T(8,128)(2,1)S(1)} %copy-done.27, bf16[1024,512]{1,0:T(8,128)(2,1)S(1)} %copy-done.25), kind=kOutput, calls=%fused_computation.82 | convolution fusion | flops 8606711808 | bytes 20971520 | tf_op jit(solution)/shard_map/dot_general | solution.py:29
  572.4 6.1 multiply_reduce_fusion
  579.4 3.9 fusion.10
  585.0 3.6 collective-permute-done.28
  589.9 2.9 collective-permute-done.29
  592.8 8.6 %collective-permute-start.30 = (f32[4,1352]{1,0:T(4,128)S(1)}, f32[4,1352]{1,0:T(4,128)S(1)}, u32[]{:S(2)}, u32[]{:S(2)}) collective-permute-start(f32[4,1352]{1,0:T(4,128)S(1)} %slice_select_fusion.2), channel_id=1, source_target_pairs={{0,4},{1,5},{2,6},{3,7},{4,0},{5,1},{6,2},{7,3},{8,12},{9,13},{10,... | collective-permute-start | bytes 64904 | tf_op jit(solution)/shard_map/ppermute | solution.py:621
  601.4 5.9 convolution_convert_fusion.6
  611.6 6.8 collective-permute-done.24
  627.5 22.0 %reduce-scatter.9.cloned.1.call-done = bf16[256,2048]{1,0:T(8,128)(2,1)} async-done(((bf16[2048,2048]{1,0:T(8,128)(2,1)}), bf16[256,2048]{1,0:T(8,128)(2,1)}) %reduce-scatter.9.cloned.1.call-update) | async-done | bytes 1048592 | tf_op jit(solution)/shard_map/reduce_scatter | solution.py:885
  649.5 2.8 fusion.4
  652.5 2.5 collective-permute-start.38
  656.0 3.7 fusion.13
  661.0 3.8 collective-permute-done.38
  664.8 4.4 collective-permute-done.37
  676.8 3.9 collective-permute-done.35
  680.8 4.6 collective-permute-done.34
  687.2 2.9 reshape.424
  (370 shorter events, 109.7 us)
Async XLA Ops:
  7.2 276.8 %all-gather.3.cloned.1.call-start = ((), (), s32[]{:S(2)}) async-start(), calls=%async_computation.4 | async-start | bytes 12976128 | tf_op jit(solution)/shard_map/all_gather | solution.py:758
  129.9 201.9 %all-gather.5.cloned.1.call-start = ((), (), s32[]{:S(2)}) async-start(), calls=%async_computation.5 | async-start | bytes 6488064 | tf_op jit(solution)/shard_map/all_gather | solution.py:764
  129.9 37.2 %collective-permute-start = (bf16[256,2048]{1,0:T(8,128)(2,1)}, bf16[256,2048]{1,0:T(8,128)(2,1)}, u32[]{:S(2)}, u32[]{:S(2)}) collective-permute-start(bf16[256,2048]{1,0:T(8,128)(2,1)} %bitcast.6), channel_id=1, source_target_pairs={{0,8},{8,0},{16,24},{24,16},{1,9},{9,1},{17,25},{25,17},{2,10},{10... | collective-permute-start | bytes 3145736 | tf_op jit(solution)/shard_map/ppermute | solution.py:589
  131.5 31.3 %collective-permute-start.1 = (bf16[256,2048]{1,0:T(8,128)(2,1)}, bf16[256,2048]{1,0:T(8,128)(2,1)}, u32[]{:S(2)}, u32[]{:S(2)}) collective-permute-start(bf16[256,2048]{1,0:T(8,128)(2,1)} %bitcast.6), channel_id=1, source_target_pairs={{0,16},{8,24},{16,0},{24,8},{1,17},{9,25},{17,1},{25,9},{2,18},{10... | collective-permute-start | bytes 3145736 | tf_op jit(solution)/shard_map/ppermute | solution.py:589
  164.7 14.2 %collective-permute-start.2 = (bf16[128,2048]{1,0:T(8,128)(2,1)}, bf16[128,2048]{1,0:T(8,128)(2,1)}, u32[]{:S(2)}, u32[]{:S(2)}) collective-permute-start(bf16[128,2048]{1,0:T(8,128)(2,1)} %slice.260), channel_id=1, source_target_pairs={{0,8},{8,0},{16,24},{24,16},{1,9},{9,1},{17,25},{25,17},{2,10},{10... | collective-permute-start | bytes 1572872 | tf_op jit(solution)/shard_map/ppermute | solution.py:589
  165.3 29.4 %copy-start.64 = (f32[512]{0:T(512)}, f32[512]{0:T(512)S(1)}, u32[]{:S(2)}) copy-start(f32[512]{0:T(512)S(1)} %dynamic-slice_convert_fusion) | copy-start | bytes 6148
  168.4 13.5 %collective-permute-start.3 = (bf16[128,2048]{1,0:T(8,128)(2,1)S(1)}, bf16[128,2048]{1,0:T(8,128)(2,1)S(1)}, u32[]{:S(2)}, u32[]{:S(2)}) collective-permute-start(bf16[128,2048]{1,0:T(8,128)(2,1)S(1)} %slice.261), channel_id=1, source_target_pairs={{0,16},{8,24},{16,0},{24,8},{1,17},{9,25},{17,1},{25,9},{2,18},{10... | collective-permute-start | bytes 1572872 | tf_op jit(solution)/shard_map/ppermute | solution.py:589
  202.1 12.7 %collective-permute-start.4 = (bf16[128,2048]{1,0:T(8,128)(2,1)S(1)}, bf16[128,2048]{1,0:T(8,128)(2,1)S(1)}, u32[]{:S(2)}, u32[]{:S(2)}) collective-permute-start(bf16[128,2048]{1,0:T(8,128)(2,1)S(1)} %get-tuple-element.160), channel_id=1, source_target_pairs={{0,16},{8,24},{16,0},{24,8},{1,17},{9,25},{17,1},{25,9},{2,18},{10... | collective-permute-start | bytes 1572872 | tf_op jit(solution)/shard_map/ppermute | solution.py:589
  202.4 12.6 %collective-permute-start.6 = (bf16[128,2048]{1,0:T(8,128)(2,1)S(1)}, bf16[128,2048]{1,0:T(8,128)(2,1)S(1)}, u32[]{:S(2)}, u32[]{:S(2)}) collective-permute-start(bf16[128,2048]{1,0:T(8,128)(2,1)S(1)} %get-tuple-element.159), channel_id=1, source_target_pairs={{0,8},{8,0},{16,24},{24,16},{1,9},{9,1},{17,25},{25,17},{2,10},{10... | collective-permute-start | bytes 1572872 | tf_op jit(solution)/shard_map/ppermute | solution.py:589
  216.5 23.4 %collective-permute-start.7 = (bf16[256,2048]{1,0:T(8,128)(2,1)}, bf16[256,2048]{1,0:T(8,128)(2,1)}, u32[]{:S(2)}, u32[]{:S(2)}) collective-permute-start(bf16[256,2048]{1,0:T(8,128)(2,1)} %pad_maximum_fusion.5), channel_id=1, source_target_pairs={{0,16},{8,24},{16,0},{24,8},{1,17},{9,25},{17,1},{25,9},{2,18},{10... | collective-permute-start | bytes 3145736 | tf_op jit(solution)/shard_map/ppermute | solution.py:589
  219.1 23.0 %collective-permute-start.5 = (bf16[256,2048]{1,0:T(8,128)(2,1)}, bf16[256,2048]{1,0:T(8,128)(2,1)}, u32[]{:S(2)}, u32[]{:S(2)}) collective-permute-start(bf16[256,2048]{1,0:T(8,128)(2,1)} %pad_maximum_fusion.4), channel_id=1, source_target_pairs={{0,8},{8,0},{16,24},{24,16},{1,9},{9,1},{17,25},{25,17},{2,10},{10... | collective-permute-start | bytes 3145736 | tf_op jit(solution)/shard_map/ppermute | solution.py:589
  220.9 27.0 %copy-start.58 = (f32[2048]{0:T(1024)}, f32[2048]{0:T(1024)S(1)}, u32[]{:S(2)}) copy-start(f32[2048]{0:T(1024)S(1)} %reshape.421) | copy-start | bytes 24580
  247.9 22.1 %collective-permute-start.9 = (bf16[256,2048]{1,0:T(8,128)(2,1)}, bf16[256,2048]{1,0:T(8,128)(2,1)}, u32[]{:S(2)}, u32[]{:S(2)}) collective-permute-start(bf16[256,2048]{1,0:T(8,128)(2,1)} %get-tuple-element.128), channel_id=1, source_target_pairs={{0,16},{8,24},{16,0},{24,8},{1,17},{9,25},{17,1},{25,9},{2,18},{10... | collective-permute-start | bytes 3145736 | tf_op jit(solution)/shard_map/ppermute | solution.py:589
  248.5 147.1 %reduce-scatter.5.cloned.1.call-start = ((), (), s32[]{:S(2)}) async-start(), calls=%async_computation.6 | async-start | bytes 6488064 | tf_op jit(solution)/shard_map/reduce_scatter | solution.py:827
  249.1 23.9 %collective-permute-start.8 = (bf16[256,2048]{1,0:T(8,128)(2,1)}, bf16[256,2048]{1,0:T(8,128)(2,1)S(1)}, u32[]{:S(2)}, u32[]{:S(2)}) collective-permute-start(bf16[256,2048]{1,0:T(8,128)(2,1)} %get-tuple-element.128), channel_id=1, source_target_pairs={{0,8},{8,0},{16,24},{24,16},{1,9},{9,1},{17,25},{25,17},{2,10},{10... | collective-permute-start | bytes 3145736 | tf_op jit(solution)/shard_map/ppermute | solution.py:589
  271.1 11.2 %collective-permute-start.10 = (bf16[128,2048]{1,0:T(8,128)(2,1)S(1)}, bf16[128,2048]{1,0:T(8,128)(2,1)S(1)}, u32[]{:S(2)}, u32[]{:S(2)}) collective-permute-start(bf16[128,2048]{1,0:T(8,128)(2,1)S(1)} %slice.273), channel_id=1, source_target_pairs={{0,8},{8,0},{16,24},{24,16},{1,9},{9,1},{17,25},{25,17},{2,10},{10... | collective-permute-start | bytes 1572872 | tf_op jit(solution)/shard_map/ppermute | solution.py:589
  273.1 10.0 %collective-permute-start.11 = (bf16[128,2048]{1,0:T(8,128)(2,1)S(1)}, bf16[128,2048]{1,0:T(8,128)(2,1)S(1)}, u32[]{:S(2)}, u32[]{:S(2)}) collective-permute-start(bf16[128,2048]{1,0:T(8,128)(2,1)S(1)} %slice.274), channel_id=1, source_target_pairs={{0,16},{8,24},{16,0},{24,8},{1,17},{9,25},{17,1},{25,9},{2,18},{10... | collective-permute-start | bytes 1572872 | tf_op jit(solution)/shard_map/ppermute | solution.py:589
  331.6 223.4 %reduce-scatter.7.cloned.1.call-start = ((), (), s32[]{:S(2)}) async-start(), calls=%async_computation.7 | async-start | bytes 12976128 | tf_op jit(solution)/shard_map/reduce_scatter | solution.py:830
  395.7 253.8 %reduce-scatter.9.cloned.1.call-start = ((), (), s32[]{:S(2)}) async-start(), calls=%async_computation.8 | async-start | bytes 9437184 | tf_op jit(solution)/shard_map/reduce_scatter | solution.py:885
  397.6 13.4 %collective-permute-start.16 = (bf16[128,2048]{1,0:T(8,128)(2,1)S(1)}, bf16[128,2048]{1,0:T(8,128)(2,1)S(1)}, u32[]{:S(2)}, u32[]{:S(2)}) collective-permute-start(bf16[128,2048]{1,0:T(8,128)(2,1)S(1)} %get-tuple-element.148), channel_id=1, source_target_pairs={{0,16},{8,24},{16,0},{24,8},{1,17},{9,25},{17,1},{25,9},{2,18},{10... | collective-permute-start | bytes 1572872 | tf_op jit(solution)/shard_map/ppermute | solution.py:589
  399.2 11.9 %collective-permute-start.18 = (bf16[128,2048]{1,0:T(8,128)(2,1)S(1)}, bf16[128,2048]{1,0:T(8,128)(2,1)S(1)}, u32[]{:S(2)}, u32[]{:S(2)}) collective-permute-start(bf16[128,2048]{1,0:T(8,128)(2,1)S(1)} %get-tuple-element.147), channel_id=1, source_target_pairs={{0,8},{8,0},{16,24},{24,16},{1,9},{9,1},{17,25},{25,17},{2,10},{10... | collective-permute-start | bytes 1572872 | tf_op jit(solution)/shard_map/ppermute | solution.py:589
  410.6 14.9 %collective-permute-start.12 = (bf16[128,2048]{1,0:T(8,128)(2,1)S(1)}, bf16[128,2048]{1,0:T(8,128)(2,1)S(1)}, u32[]{:S(2)}, u32[]{:S(2)}) collective-permute-start(bf16[128,2048]{1,0:T(8,128)(2,1)S(1)} %get-tuple-element.154), channel_id=1, source_target_pairs={{0,16},{8,24},{16,0},{24,8},{1,17},{9,25},{17,1},{25,9},{2,18},{10... | collective-permute-start | bytes 1572872 | tf_op jit(solution)/shard_map/ppermute | solution.py:589
  410.7 14.9 %collective-permute-start.14 = (bf16[128,2048]{1,0:T(8,128)(2,1)S(1)}, bf16[128,2048]{1,0:T(8,128)(2,1)S(1)}, u32[]{:S(2)}, u32[]{:S(2)}) collective-permute-start(bf16[128,2048]{1,0:T(8,128)(2,1)S(1)} %get-tuple-element.153), channel_id=1, source_target_pairs={{0,8},{8,0},{16,24},{24,16},{1,9},{9,1},{17,25},{25,17},{2,10},{10... | collective-permute-start | bytes 1572872 | tf_op jit(solution)/shard_map/ppermute | solution.py:589
  413.3 34.8 %collective-permute-start.19 = (bf16[256,2048]{1,0:T(8,128)(2,1)S(1)}, bf16[256,2048]{1,0:T(8,128)(2,1)S(1)}, u32[]{:S(2)}, u32[]{:S(2)}) collective-permute-start(bf16[256,2048]{1,0:T(8,128)(2,1)S(1)} %pad_maximum_fusion.9), channel_id=1, source_target_pairs={{0,16},{8,24},{16,0},{24,8},{1,17},{9,25},{17,1},{25,9},{2,18},{10... | collective-permute-start | bytes 3145736 | tf_op jit(solution)/shard_map/ppermute | solution.py:589
  413.5 53.1 %copy-start.34 = (f32[256,2048]{1,0:T(8,128)S(1)}, f32[256,2048]{1,0:T(8,128)}, u32[]{:S(2)}) copy-start(f32[256,2048]{1,0:T(8,128)} %copy-done.33) | copy-start | bytes 6291460
  413.5 53.1 %copy-start.59 = (f32[2048]{0:T(1024)S(1)}, f32[2048]{0:T(1024)}, u32[]{:S(2)}) copy-start(f32[2048]{0:T(1024)} %copy-done.58) | copy-start | bytes 24580
  413.5 53.1 %copy-start.69 = (f32[256]{0:T(256)S(1)}, f32[256]{0:T(256)}, u32[]{:S(2)}) copy-start(f32[256]{0:T(256)} %copy-done.68) | copy-start | bytes 3076
  413.5 34.6 %collective-permute-start.17 = (bf16[256,2048]{1,0:T(8,128)(2,1)S(1)}, bf16[256,2048]{1,0:T(8,128)(2,1)S(1)}, u32[]{:S(2)}, u32[]{:S(2)}) collective-permute-start(bf16[256,2048]{1,0:T(8,128)(2,1)S(1)} %pad_maximum_fusion.8), channel_id=1, source_target_pairs={{0,8},{8,0},{16,24},{24,16},{1,9},{9,1},{17,25},{25,17},{2,10},{10... | collective-permute-start | bytes 3145736 | tf_op jit(solution)/shard_map/ppermute | solution.py:589
  426.1 39.7 %collective-permute-start.15 = (bf16[256,2048]{1,0:T(8,128)(2,1)S(1)}, bf16[256,2048]{1,0:T(8,128)(2,1)S(1)}, u32[]{:S(2)}, u32[]{:S(2)}) collective-permute-start(bf16[256,2048]{1,0:T(8,128)(2,1)S(1)} %pad_maximum_fusion.7), channel_id=1, source_target_pairs={{0,16},{8,24},{16,0},{24,8},{1,17},{9,25},{17,1},{25,9},{2,18},{10... | collective-permute-start | bytes 3145736 | tf_op jit(solution)/shard_map/ppermute | solution.py:589
  428.2 40.8 %copy-start.70 = (f32[256]{0:T(256)S(1)}, f32[256]{0:T(256)}, u32[]{:S(2)}) copy-start(f32[256]{0:T(256)} %get-tuple-element.209) | copy-start | bytes 3076
  428.3 38.3 %collective-permute-start.13 = (bf16[256,2048]{1,0:T(8,128)(2,1)S(1)}, bf16[256,2048]{1,0:T(8,128)(2,1)S(1)}, u32[]{:S(2)}, u32[]{:S(2)}) collective-permute-start(bf16[256,2048]{1,0:T(8,128)(2,1)S(1)} %pad_maximum_fusion.6), channel_id=1, source_target_pairs={{0,8},{8,0},{16,24},{24,16},{1,9},{9,1},{17,25},{25,17},{2,10},{10... | collective-permute-start | bytes 3145736 | tf_op jit(solution)/shard_map/ppermute | solution.py:589
  469.1 38.1 %slice-start = ((s8[8388608]{0:T(1024)(128)(4,1)}), s8[4194304]{0:T(1024)(128)(4,1)S(1)}, s32[]{:S(2)}) async-start(s8[8388608]{0:T(1024)(128)(4,1)} %bitcast.187), calls=%async_computation.10 | async-start | bytes 8388608
  469.1 28.3 %copy-start.67 = (f32[1,2,4,128]{3,2,1,0:T(4,128)S(1)}, f32[1,2,4,128]{3,2,1,0:T(4,128)}, u32[]{:S(2)}) copy-start(f32[1,2,4,128]{3,2,1,0:T(4,128)} %get-tuple-element.200) | copy-start | bytes 12292
  469.1 38.1 %slice-start.1 = ((s8[8388608]{0:T(1024)(128)(4,1)}), s8[4194304]{0:T(1024)(128)(4,1)S(1)}, s32[]{:S(2)}) async-start(s8[8388608]{0:T(1024)(128)(4,1)} %bitcast.187), calls=%async_computation.11 | async-start | bytes 8388608
  472.8 34.4 %copy-start.1 = (f32[1024,512]{1,0:T(8,128)S(1)}, f32[1024,512]{1,0:T(8,128)}, u32[]{:S(2)}) copy-start(f32[1024,512]{1,0:T(8,128)} %copy-done) | copy-start | bytes 6291460
  472.8 34.4 %copy-start.63 = (f32[1024]{0:T(1024)S(1)}, f32[1024]{0:T(1024)}, u32[]{:S(2)}) copy-start(f32[1024]{0:T(1024)} %copy-done.62) | copy-start | bytes 12292
  472.8 34.5 %copy-start.65 = (f32[512]{0:T(512)S(1)}, f32[512]{0:T(512)}, u32[]{:S(2)}) copy-start(f32[512]{0:T(512)} %copy-done.64) | copy-start | bytes 6148
  472.8 34.5 %copy-start.73 = (bf16[8,64,2048]{2,1,0:T(8,128)(2,1)S(1)}, bf16[8,64,2048]{2,1,0:T(8,128)(2,1)}, u32[]{:S(2)}) copy-start(bf16[8,64,2048]{2,1,0:T(8,128)(2,1)} %get-tuple-element.48) | copy-start | bytes 6291460
  472.8 21.4 %collective-permute-start.21 = (bf16[256,2048]{1,0:T(8,128)(2,1)S(1)}, bf16[256,2048]{1,0:T(8,128)(2,1)S(1)}, u32[]{:S(2)}, u32[]{:S(2)}) collective-permute-start(bf16[256,2048]{1,0:T(8,128)(2,1)S(1)} %get-tuple-element.125), channel_id=1, source_target_pairs={{0,16},{8,24},{16,0},{24,8},{1,17},{9,25},{17,1},{25,9},{2,18},{10... | collective-permute-start | bytes 3145736 | tf_op jit(solution)/shard_map/ppermute | solution.py:589
  473.9 23.5 %collective-permute-start.20 = (bf16[256,2048]{1,0:T(8,128)(2,1)S(1)}, bf16[256,2048]{1,0:T(8,128)(2,1)S(1)}, u32[]{:S(2)}, u32[]{:S(2)}) collective-permute-start(bf16[256,2048]{1,0:T(8,128)(2,1)S(1)} %get-tuple-element.125), channel_id=1, source_target_pairs={{0,8},{8,0},{16,24},{24,16},{1,9},{9,1},{17,25},{25,17},{2,10},{10... | collective-permute-start | bytes 3145736 | tf_op jit(solution)/shard_map/ppermute | solution.py:589
  494.2 12.3 %collective-permute-start.22 = (bf16[128,2048]{1,0:T(8,128)(2,1)S(1)}, bf16[128,2048]{1,0:T(8,128)(2,1)S(1)}, u32[]{:S(2)}, u32[]{:S(2)}) collective-permute-start(bf16[128,2048]{1,0:T(8,128)(2,1)S(1)} %slice.291), channel_id=1, source_target_pairs={{0,8},{8,0},{16,24},{24,16},{1,9},{9,1},{17,25},{25,17},{2,10},{10... | collective-permute-start | bytes 1572872 | tf_op jit(solution)/shard_map/ppermute | solution.py:589
  497.4 9.7 %collective-permute-start.23 = (bf16[128,2048]{1,0:T(8,128)(2,1)S(1)}, bf16[128,2048]{1,0:T(8,128)(2,1)S(1)}, u32[]{:S(2)}, u32[]{:S(2)}) collective-permute-start(bf16[128,2048]{1,0:T(8,128)(2,1)S(1)} %slice.292), channel_id=1, source_target_pairs={{0,16},{8,24},{16,0},{24,8},{1,17},{9,25},{17,1},{25,9},{2,18},{10... | collective-permute-start | bytes 1572872 | tf_op jit(solution)/shard_map/ppermute | solution.py:589
  512.3 21.9 %copy-start.45 = (bf16[1024,512]{1,0:T(8,128)(2,1)}, bf16[1024,512]{1,0:T(8,128)(2,1)S(1)}, u32[]{:S(2)}) copy-start(bf16[1024,512]{1,0:T(8,128)(2,1)S(1)} %get-tuple-element.132) | copy-start | bytes 3145732
  512.7 21.5 %copy-start.31 = (bf16[4,256,2048]{2,1,0:T(8,128)(2,1)S(1)}, bf16[4,256,2048]{2,1,0:T(8,128)(2,1)}, u32[]{:S(2)}) copy-start(bf16[4,256,2048]{2,1,0:T(8,128)(2,1)} %get-tuple-element.42) | copy-start | bytes 12582916
  512.7 21.5 %copy-start.57 = (f32[2048]{0:T(1024)S(1)}, f32[2048]{0:T(1024)}, u32[]{:S(2)}) copy-start(f32[2048]{0:T(1024)} %copy-done.56) | copy-start | bytes 24580
  555.0 142.1 %reduce-scatter.11.cloned.1.call-start = ((), (), s32[]{:S(2)}) async-start(), calls=%async_computation.9 | async-start | bytes 2359296 | tf_op jit(solution)/shard_map/reduce_scatter | solution.py:886
  579.4 22.1 %copy-start.48 = (bf16[1024,512]{1,0:T(8,128)(2,1)S(1)}, bf16[1024,512]{1,0:T(8,128)(2,1)}, u32[]{:S(2)}) copy-start(bf16[1024,512]{1,0:T(8,128)(2,1)} %copy-done.47) | copy-start | bytes 3145732
  584.1 4.6 collective-permute-start.28
  588.7 4.1 collective-permute-start.29
  592.8 14.5 %collective-permute-start.30 = (f32[4,1352]{1,0:T(4,128)S(1)}, f32[4,1352]{1,0:T(4,128)S(1)}, u32[]{:S(2)}, u32[]{:S(2)}) collective-permute-start(f32[4,1352]{1,0:T(4,128)S(1)} %slice_select_fusion.2), channel_id=1, source_target_pairs={{0,4},{1,5},{2,6},{3,7},{4,0},{5,1},{6,2},{7,3},{8,12},{9,13},{10,... | collective-permute-start | bytes 64904 | tf_op jit(solution)/shard_map/ppermute | solution.py:621
  607.4 4.2 collective-permute-start.31
  609.1 9.3 %collective-permute-start.24 = (bf16[128,2048]{1,0:T(8,128)(2,1)S(1)}, bf16[128,2048]{1,0:T(8,128)(2,1)S(1)}, u32[]{:S(2)}, u32[]{:S(2)}) collective-permute-start(bf16[128,2048]{1,0:T(8,128)(2,1)S(1)} %get-tuple-element.142), channel_id=1, source_target_pairs={{0,16},{8,24},{16,0},{24,8},{1,17},{9,25},{17,1},{25,9},{2,18},{10... | collective-permute-start | bytes 1572872 | tf_op jit(solution)/shard_map/ppermute | solution.py:589
  609.3 9.6 %collective-permute-start.26 = (bf16[128,2048]{1,0:T(8,128)(2,1)S(1)}, bf16[128,2048]{1,0:T(8,128)(2,1)S(1)}, u32[]{:S(2)}, u32[]{:S(2)}) collective-permute-start(bf16[128,2048]{1,0:T(8,128)(2,1)S(1)} %get-tuple-element.141), channel_id=1, source_target_pairs={{0,8},{8,0},{16,24},{24,16},{1,9},{9,1},{17,25},{25,17},{2,10},{10... | collective-permute-start | bytes 1572872 | tf_op jit(solution)/shard_map/ppermute | solution.py:589
  611.5 37.9 %copy-start.36 = (bf16[1,256,2048]{2,1,0:T(8,128)(2,1)S(1)}, bf16[1,256,2048]{2,1,0:T(8,128)(2,1)}, u32[]{:S(2)}) copy-start(bf16[1,256,2048]{2,1,0:T(8,128)(2,1)} %param.24) | copy-start | bytes 3145732
  611.6 13.1 %collective-permute-start.32 = (f32[1,1352]{1,0:T(1,128)S(1)}, f32[1,1352]{1,0:T(1,128)S(1)}, u32[]{:S(2)}, u32[]{:S(2)}) collective-permute-start(f32[1,1352]{1,0:T(1,128)S(1)} %broadcast_select_fusion.1), channel_id=1, source_target_pairs={{0,1},{1,0},{2,3},{3,2},{4,5},{5,4},{6,7},{7,6},{8,9},{9,8},{10,11... | collective-permute-start | bytes 16232 | tf_op jit(solution)/shard_map/ppermute | solution.py:621
  621.5 28.0 %collective-permute-start.27 = (bf16[256,2048]{1,0:T(8,128)(2,1)}, bf16[256,2048]{1,0:T(8,128)(2,1)}, u32[]{:S(2)}, u32[]{:S(2)}) collective-permute-start(bf16[256,2048]{1,0:T(8,128)(2,1)} %pad_maximum_fusion.11), channel_id=1, source_target_pairs={{0,16},{8,24},{16,0},{24,8},{1,17},{9,25},{17,1},{25,9},{2,18},{10... | collective-permute-start | bytes 3145736 | tf_op jit(solution)/shard_map/ppermute | solution.py:589
  624.1 25.4 %collective-permute-start.25 = (bf16[256,2048]{1,0:T(8,128)(2,1)}, bf16[256,2048]{1,0:T(8,128)(2,1)}, u32[]{:S(2)}, u32[]{:S(2)}) collective-permute-start(bf16[256,2048]{1,0:T(8,128)(2,1)} %pad_maximum_fusion.10), channel_id=1, source_target_pairs={{0,8},{8,0},{16,24},{24,16},{1,9},{9,1},{17,25},{25,17},{2,10},{10... | collective-permute-start | bytes 3145736 | tf_op jit(solution)/shard_map/ppermute | solution.py:589
  627.5 28.6 %copy-start.37 = (f32[256,2048]{1,0:T(8,128)S(1)}, f32[256,2048]{1,0:T(8,128)}, u32[]{:S(2)}) copy-start(f32[256,2048]{1,0:T(8,128)} %get-tuple-element.126) | copy-start | bytes 6291460
  652.5 12.3 %collective-permute-start.38 = (bf16[2,64,1408]{2,1,0:T(8,128)(2,1)S(1)}, bf16[2,64,1408]{2,1,0:T(8,128)(2,1)S(1)}, u32[]{:S(2)}, u32[]{:S(2)}) collective-permute-start(bf16[2,64,1408]{2,1,0:T(8,128)(2,1)S(1)} %get-tuple-element.178), channel_id=1, source_target_pairs={{0,24},{8,16},{16,8},{24,0},{1,25},{9,17},{17,9},{25,1},{2,26},{10... | collective-permute-start | bytes 1081352 | tf_op jit(solution)/shard_map/ppermute | solution.py:589
  654.9 14.2 %collective-permute-start.37 = (bf16[2,64,1408]{2,1,0:T(8,128)(2,1)S(1)}, bf16[2,64,1408]{2,1,0:T(8,128)(2,1)S(1)}, u32[]{:S(2)}, u32[]{:S(2)}) collective-permute-start(bf16[2,64,1408]{2,1,0:T(8,128)(2,1)S(1)} %get-tuple-element.179), channel_id=1, source_target_pairs={{0,16},{8,24},{16,0},{24,8},{1,17},{9,25},{17,1},{25,9},{2,18},{10... | collective-permute-start | bytes 1081352 | tf_op jit(solution)/shard_map/ppermute | solution.py:589
  655.5 13.8 %collective-permute-start.36 = (bf16[2,64,1408]{2,1,0:T(8,128)(2,1)S(1)}, bf16[2,64,1408]{2,1,0:T(8,128)(2,1)S(1)}, u32[]{:S(2)}, u32[]{:S(2)}) collective-permute-start(bf16[2,64,1408]{2,1,0:T(8,128)(2,1)S(1)} %get-tuple-element.180), channel_id=1, source_target_pairs={{0,8},{8,0},{16,24},{24,16},{1,9},{9,1},{17,25},{25,17},{2,10},{10... | collective-permute-start | bytes 1081352 | tf_op jit(solution)/shard_map/ppermute | solution.py:589
  670.6 10.2 %collective-permute-start.35 = (bf16[64,2048]{1,0:T(8,128)(2,1)S(1)}, bf16[64,2048]{1,0:T(8,128)(2,1)S(1)}, u32[]{:S(2)}, u32[]{:S(2)}) collective-permute-start(bf16[64,2048]{1,0:T(8,128)(2,1)S(1)} %get-tuple-element.186), channel_id=1, source_target_pairs={{0,24},{8,16},{16,8},{24,0},{1,25},{9,17},{17,9},{25,1},{2,26},{10... | collective-permute-start | bytes 786440 | tf_op jit(solution)/shard_map/ppermute | solution.py:589
  672.3 13.0 %collective-permute-start.34 = (bf16[64,2048]{1,0:T(8,128)(2,1)S(1)}, bf16[64,2048]{1,0:T(8,128)(2,1)S(1)}, u32[]{:S(2)}, u32[]{:S(2)}) collective-permute-start(bf16[64,2048]{1,0:T(8,128)(2,1)S(1)} %get-tuple-element.187), channel_id=1, source_target_pairs={{0,16},{8,24},{16,0},{24,8},{1,17},{9,25},{17,1},{25,9},{2,18},{10... | collective-permute-start | bytes 786440 | tf_op jit(solution)/shard_map/ppermute | solution.py:589
  673.6 11.9 %collective-permute-start.33 = (bf16[64,2048]{1,0:T(8,128)(2,1)S(1)}, bf16[64,2048]{1,0:T(8,128)(2,1)S(1)}, u32[]{:S(2)}, u32[]{:S(2)}) collective-permute-start(bf16[64,2048]{1,0:T(8,128)(2,1)S(1)} %get-tuple-element.188), channel_id=1, source_target_pairs={{0,8},{8,0},{16,24},{24,16},{1,9},{9,1},{17,25},{25,17},{2,10},{10... | collective-permute-start | bytes 786440 | tf_op jit(solution)/shard_map/ppermute | solution.py:589
  (62 other events, 415.8 us)
Sparse Core Ops, SparseCore 0:
  130.0 108.2 all-gather.2
  248.6 59.8 all-gather.4
  331.7 63.8 reduce-scatter.4
  397.8 117.6 reduce-scatter.6
  555.1 94.2 reduce-scatter.8
  651.6 33.9 reduce-scatter.10

commit v4 on v3

--- a/solution.py
+++ b/solution.py
@@ -463,16 +463,17 @@
 
 
 def start_kernel(
-    ring, lines, inputs, w_query, w_key, w_value, w_swish, w_out, gate, up, small,
-    inputs_all, w_mixer, w_output, feed_columns, small_all, local_sem, send_sem, recv_sem,
+    ring, lines, inputs, cotangent, w_query, w_key, w_value, w_swish, w_out, gate, up, small,
+    inputs_all, cotangent_all, w_mixer, swish_columns, out_rows, feed_columns, small_all,
+    local_sem, send_sem, recv_sem,
 ):
     mine, batch = lax.axis_index("seq"), lax.axis_index("batch")
     chips = lines // 2
     copies = Copies(local_sem, send_sem, recv_sem)
-    part = w_mixer.shape[3] // 4
+    part = swish_columns.shape[2]
     half = inputs.shape[0] // 2
     others = peers(ring, mine)
-    pieces = (w_query, w_key, w_value, w_swish)
+    pieces = (w_query, w_key, w_value)
 
     def column(ref, at):
         if len(ref.shape) == 3:
@@ -484,7 +485,7 @@
         return w_mixer.at[source, batch, :, pl.ds(piece * part, part)]
 
     near = [copies.near(column(ref, mine), slot(mine, at)) for at, ref in enumerate(pieces)]
-    near += [copies.near(w_out, w_output.at[batch]), copies.near(small, small_all.at[mine, batch])]
+    near += [copies.near(small, small_all.at[mine, batch])]
     column_waits, small_waits = [], []
     for to in others:
         column_waits.append(
@@ -496,12 +497,26 @@
         small_waits.append(
             copies.far(small, small_all.at[mine, batch], small_all.at[to, batch], (to, batch))
         )
-    own_input = copies.near(inputs, inputs_all.at[0])
     direct = 2 if ring == 4 else ring - 1
-    input_waits = [
-        copies.far(inputs, inputs_all.at[by + 1], inputs_all.at[by + 1], (others[by], batch))
-        for by in range(direct)
-    ]
+
+    def sent(block, blocks):
+        return copies.near(block, blocks.at[0]), [
+            copies.far(block, blocks.at[by + 1], blocks.at[by + 1], (others[by], batch))
+            for by in range(direct)
+        ]
+
+    def passed_on(blocks, waits):
+        for wait in waits:
+            wait()
+        if ring != 4:
+            return []
+        low, high = pl.ds(0, half), pl.ds(half, half)
+        return [
+            copies.far(blocks.at[have, rows], blocks.at[3, rows], blocks.at[3, rows], (to, batch))
+            for have, rows, to in ((2, low, others[0]), (1, high, others[1]))
+        ]
+
+    own_input, input_waits = sent(inputs, inputs_all)
     for copy in near:
         copy.wait()
 
@@ -520,65 +535,198 @@
         wait()
         started(lambda at, source=source: small_all.at[source, at])
     started(lambda at: small_all.at[mine, at])
-    started(lambda at: w_output.at[at])
-    own_feed = [copies.near(column(ref, mine), feed_columns.at[at, mine]) for at, ref in enumerate((gate, up))]
-    for chain in chains:
-        if chips > 1:
-            next(chain)
-    if ring == 4:
-        for wait in input_waits:
-            wait()
-        low, high = pl.ds(0, half), pl.ds(half, half)
-        input_waits = [
-            copies.far(
-                inputs_all.at[have, rows], inputs_all.at[3, rows], inputs_all.at[3, rows], (to, batch)
-            )
-            for have, rows, to in ((2, low, others[0]), (1, high, others[1]))
-        ]
-    feed_waits = [
+    input_waits = passed_on(inputs_all, input_waits)
+    own_columns = [
+        copies.near(column(w_swish, mine), swish_columns.at[mine]),
+        copies.near(w_out, out_rows),
+    ]
+    own_columns += [
+        copies.near(column(ref, mine), feed_columns.at[at, mine]) for at, ref in enumerate((gate, up))
+    ]
+    other_waits = [
+        copies.far(column(w_swish, to), swish_columns.at[mine], swish_columns.at[to], (to, batch))
+        for to in others
+    ]
+    other_waits += [
         copies.far(
             column(ref, to), feed_columns.at[at, mine], feed_columns.at[at, to], (to, batch)
         )
         for to in others
         for at, ref in enumerate((gate, up))
     ]
-    for _ in range(chips - 1 if chips > 1 else 1):
+    own_cotangent, cotangent_waits = sent(cotangent, cotangent_all)
+    for step in range(1, chips + 1):
+        for chain in chains:
+            if chips > 1 or step > 1:
+                next(chain)
+        if step == min(2, chips):
+            cotangent_waits = passed_on(cotangent_all, cotangent_waits)
+    if chips == 1:
         for chain in chains:
             next(chain)
-    for wait in input_waits + feed_waits:
+    for wait in input_waits + cotangent_waits + other_waits:
         wait()
-    for copy in [own_input] + own_feed:
+    for copy in [own_input, own_cotangent] + own_columns:
         copy.wait()
     copies.close()
 
 
-def start(ring, lines, inputs, columns, w_out, gate, up, small):
+def start(ring, lines, inputs, cotangent, columns, w_out, gate, up, small):
     own, width = columns[0].shape
     part, hidden = width // ring, gate.shape[1] // ring
     if hidden % 128:
         gate, up = (a.reshape(own, ring, hidden).transpose(1, 0, 2) for a in (gate, up))
-    chains = 2 * ring + 1
-    away = (ring - 1) * 8 + 4 + chains * (4 * (lines // 2 - 1) + 1)
-    anywhere = pl.BlockSpec(memory_space=pl.ANY)
+    chains = 2 * ring
+    away = (ring - 1) * 9 + 4 + chains * (4 * (lines // 2 - 1) + 1)
+    gathered_shape = jax.ShapeDtypeStruct((ring,) + inputs.shape, BF16)
     return pl.pallas_call(
         functools.partial(start_kernel, ring, lines),
         out_shape=(
-            jax.ShapeDtypeStruct((ring,) + inputs.shape, BF16),
-            jax.ShapeDtypeStruct((ring, lines, own, 4 * part), BF16),
-            jax.ShapeDtypeStruct((lines,) + w_out.shape, BF16),
+            gathered_shape,
+            gathered_shape,
+            jax.ShapeDtypeStruct((ring, lines, own, 3 * part), BF16),
+            jax.ShapeDtypeStruct((ring, own, part), BF16),
+            jax.ShapeDtypeStruct(w_out.shape, BF16),
             jax.ShapeDtypeStruct((2, ring, own, hidden), BF16),
             jax.ShapeDtypeStruct((ring, lines) + small.shape, BF16),
         ),
-        in_specs=[anywhere] * 9,
-        out_specs=[anywhere] * 5,
+        in_specs=[pl.BlockSpec(memory_space=pltpu.VMEM)] * 10,
+        out_specs=[pl.BlockSpec(memory_space=pl.ANY)] * 7,
         scratch_shapes=[
             pltpu.SemaphoreType.DMA((12,)),
             pltpu.SemaphoreType.DMA((away,)),
             pltpu.SemaphoreType.DMA((away,)),
         ],
-        compiler_params=pltpu.CompilerParams(has_side_effects=True),
+        compiler_params=pltpu.CompilerParams(has_side_effects=True, vmem_limit_bytes=32 << 20),
         name="start",
-    )(inputs, *columns, w_out, gate, up, small)
+    )(inputs, cotangent, *columns, w_out, gate, up, small)
+
+
+PARTS = 4
+
+
+def fold_kernel(finish, extras, *refs):
+    terms, given = refs[0], refs[1 : 1 + extras]
+    blocks = refs[1 + extras]
+    made = refs[2 + extras : -9]
+    first, second, third, two_low, one_high, own, local_sem, send_sem, recv_sem = refs[-9:]
+    mine, batch = lax.axis_index("seq"), lax.axis_index("batch")
+    others = peers(4, mine)
+    row, col = (others[0], batch), (others[1], batch)
+    copies = Copies(local_sem, send_sem, recv_sem)
+    size = terms.shape[1] // PARTS
+
+    def span(at):
+        low = pl.ds(at * size, size // 2)
+        return pl.ds(at * size, size), low, pl.ds(at * size + size // 2, size // 2)
+
+    opening, direct = [], []
+
+    def open_part(at):
+        _, low, high = span(at)
+        opening.append(
+            (
+                copies.far(terms.at[3, low], first.at[low], first.at[low], row),
+                copies.far(terms.at[3, high], first.at[high], first.at[high], col),
+            )
+        )
+
+    def pass_part(at):
+        _, low, high = span(at)
+        waits = [
+            copies.far(terms.at[2, high], second.at[high], second.at[high], col),
+            copies.far(terms.at[1, low], third.at[low], third.at[low], row),
+        ]
+        opening[at][0]()
+        two_low[low, :] = added(terms[2, low, :], first[low, :])
+        waits.append(copies.far(two_low.at[low], second.at[low], second.at[low], col))
+        opening[at][1]()
+        one_high[high, :] = added(terms[1, high, :], first[high, :])
+        waits.append(copies.far(one_high.at[high], third.at[high], third.at[high], row))
+        direct.append(waits)
+
+    spread, local, passed = [], [], []
+
+    def close_part(at):
+        full, _, _ = span(at)
+        for wait in direct[at]:
+            wait()
+        total = terms[0, full, :].astype(F32) + second[full, :].astype(F32) + third[full, :].astype(F32)
+        own[full, :] = finish(total, full, at, given, made)
+        spread.append(
+            (
+                copies.far(own.at[full], blocks.at[1, full], blocks.at[1, full], row),
+                copies.far(own.at[full], blocks.at[2, full], blocks.at[2, full], col),
+            )
+        )
+        local.append(copies.near(own.at[full], blocks.at[0, full]))
+
+    def forward_part(at):
+        _, low, high = span(at)
+        for wait in spread[at]:
+            wait()
+        passed.append(copies.far(blocks.at[2, low], blocks.at[3, low], blocks.at[3, low], row))
+        passed.append(copies.far(blocks.at[1, high], blocks.at[3, high], blocks.at[3, high], col))
+
+    open_part(0)
+    for at in range(PARTS + 2):
+        if at + 1 < PARTS:
+            open_part(at + 1)
+        if at < PARTS:
+            pass_part(at)
+        if 1 <= at <= PARTS:
+            close_part(at - 1)
+        if at >= 2:
+            forward_part(at - 2)
+    for wait in passed:
+        wait()
+    for copy in local:
+        copy.wait()
+    copies.close()
+
+
+def finish_forward(total, full, at, given, made):
+    inputs, gain = given
+    hidden = inputs[full, :].astype(F32) + total
+    made[0][full, :] = hidden
+    return (hidden * rms_scale(hidden) * gain[...]).astype(BF16)
+
+
+def finish_backward(total, full, at, given, made):
+    cotangent, hidden_ref, gain = given
+    hidden = hidden_ref[full, :]
+    scale = rms_scale(hidden)
+    plain = hidden * scale
+    term = jnp.sum(total * plain, axis=0, keepdims=True)
+    made[1][...] = term if at == 0 else made[1][...] + term
+    scaled = total * gain[...]
+    grad = (
+        cotangent[full, :].astype(F32)
+        + scale * scaled
+        - plain * (scale * jnp.mean(scaled * plain, axis=-1, keepdims=True))
+    )
+    made[0][full, :] = grad
+    return grad.astype(BF16)
+
+
+def fold(finish, terms, given, made, name):
+    ring, rows, width = terms.shape
+    inside = pl.BlockSpec(memory_space=pltpu.VMEM)
+    block = pltpu.VMEM((rows, width), BF16)
+    return pl.pallas_call(
+        functools.partial(fold_kernel, finish, len(given)),
+        out_shape=(jax.ShapeDtypeStruct((ring, rows, width), BF16),) + made,
+        in_specs=[inside] * (1 + len(given)),
+        out_specs=[pl.BlockSpec(memory_space=pl.ANY)] + [inside] * len(made),
+        scratch_shapes=[block] * 6
+        + [
+            pltpu.SemaphoreType.DMA((PARTS,)),
+            pltpu.SemaphoreType.DMA((PARTS * 10,)),
+            pltpu.SemaphoreType.DMA((PARTS * 10,)),
+        ],
+        compiler_params=pltpu.CompilerParams(has_side_effects=True, vmem_limit_bytes=40 << 20),
+        name=name,
+    )(terms, *given)
 
 
 def rms_scale(features):
@@ -724,10 +872,12 @@
     params = jnp.concatenate([params, segments.reshape(rows).astype(BF16)])
     params = jnp.pad(params, (0, -params.shape[0] % 2048)).reshape(-1, 128)
     input_own = layer_input.reshape(rows, width)
-    inputs, w_mixer, w_output, feed_columns, small = start(
+    grad_own = cotangent.reshape(rows, width)
+    inputs, grad_out, w_mixer, swish_columns, out_rows, feed_columns, small = start(
         ring,
         lines,
         input_own,
+        grad_own,
         (query_weight, key_weight, value_weight, swish_weight),
         output_weight,
         gate_weight,
@@ -735,8 +885,8 @@
         params,
     )
     inputs = inputs.reshape(length, width)
-    w_mixer = w_mixer.reshape(width, 4 * part)
-    w_output = w_output.reshape(part, width)
+    grad_out = grad_out.reshape(length, width)
+    w_mixer = w_mixer.reshape(width, 3 * part)
     small = small.reshape(devices, -1)
     segment = lax.dynamic_index_in_dim(
         small.reshape(ring, lines, -1), lax.axis_index("batch"), 1, keepdims=False
@@ -755,13 +905,16 @@
     )
     w_squeeze = w_squeeze.reshape(width, RANK).T
 
-    feed_blocks = lax.all_gather(
-        feed_columns.reshape(2 * ring * own, hidden_part), "batch", axis=0, tiled=False
-    )
-    feed_blocks = feed_blocks.reshape(lines, 2, ring, own, hidden_part)
-    feed_blocks = feed_blocks.transpose(1, 2, 0, 3, 4).reshape(2, width, hidden_part)
-    w_gate, w_up = feed_blocks[0], feed_blocks[1]
-    w_down = lax.all_gather(after(down_weight, inputs), "batch", axis=0, tiled=True)
+    def over_batch(blocks):
+        kinds, columns = blocks.shape[0], blocks.shape[-1]
+        full = lax.all_gather(blocks.reshape(-1, columns), "batch", axis=0, tiled=False)
+        full = full.reshape(lines, kinds, ring, own, columns)
+        return full.transpose(1, 2, 0, 3, 4).reshape(kinds, width, columns)
+
+    w_swish = over_batch(swish_columns[None])[0]
+    w_output = lax.all_gather(after(out_rows, w_swish), "batch", axis=0, tiled=True)
+    w_gate, w_up = over_batch(after(feed_columns, w_output))
+    w_down = lax.all_gather(after(down_weight, w_output), "batch", axis=0, tiled=True)
 
     chunked = segment.reshape(-1, CHUNK)
     before = jnp.concatenate([jnp.full((1,), -1.0, F32), chunked[:-1, -1]])
@@ -777,8 +930,6 @@
     )
     segment_col = segment[:, None]
 
-    grad_own = cotangent.reshape(rows, width)
-    grad_out = gathered(after(grad_own, inputs), ring)
     inputs = inputs.astype(F32)
     scale_one = rms_scale(inputs)
     plain_one = inputs * scale_one
@@ -787,13 +938,12 @@
     query = whole_head(mixer_pre[:, :part].astype(BF16))
     key = whole_head(mixer_pre[:, part : 2 * part].astype(BF16))
     value = whole_head(mixer_pre[:, 2 * part : 3 * part].astype(BF16))
-    swish_pre = whole_head(mixer_pre[:, 3 * part :])
+    swish_pre = whole_head(dot_nn(normed, w_swish))
     reduced = dot_nt(normed, w_squeeze).astype(BF16)
     forget_logit = dot_nt(expand_head, reduced) + bias_head.astype(F32)[:, None]
     log_rate = jax.nn.log_sigmoid(forget_logit) / TAU_GATE
     inflow = -jnp.expm1(log_rate)
     order = mine.reshape(1).astype(jnp.int32)
-    query, grad_out = lax.optimization_barrier((query, grad_out))
     mixed, attention, logits, key_start, value_start = mixer_forward(
         order, ring, query, key, value, log_rate, inflow, mask_rows, segment_col
     )
@@ -803,10 +953,20 @@
     swish_sig = jax.nn.sigmoid(swish_pre)
     swish_act = swish_pre * swish_sig
     gated = own_part((head_normed * swish_act).astype(BF16))
-    hidden = input_own.astype(F32) + scattered(dot_nn(gated, w_output).astype(BF16), ring)
-
-    scale_two = rms_scale(hidden)
-    feed_in = gathered(((hidden * scale_two * gain_two).astype(BF16)), ring)
+    terms = dot_nn(gated, w_output).astype(BF16)
+    if ring == 4:
+        feed_in, hidden = fold(
+            finish_forward,
+            terms.reshape(ring, rows, width),
+            (input_own, gain_two[None]),
+            (jax.ShapeDtypeStruct((rows, width), F32),),
+            "fold_forward",
+        )
+        feed_in = feed_in.reshape(length, width)
+    else:
+        hidden = input_own.astype(F32) + scattered(terms, ring)
+        feed_in = gathered((hidden * rms_scale(hidden) * gain_two).astype(BF16), ring)
+
     gate_pre, up_pre = dot_nn(feed_in, w_gate), dot_nn(feed_in, w_up)
     gate_sig = jax.nn.sigmoid(gate_pre)
     gate_act = gate_pre * gate_sig
@@ -818,15 +978,15 @@
     grad_gatepre = grad_gatepre.astype(BF16)
     grad_uppre = (grad_inner * gate_act).astype(BF16)
     back_feedin = (dot_nt(grad_gatepre, w_gate) + dot_nt(grad_uppre, w_up)).astype(BF16)
-    grad_feedin = scattered(back_feedin, ring)
-    feed_rows = after(feed_in, back_feedin)
-    term_gate = dot_tn(feed_rows, grad_gatepre).astype(BF16)
-    term_up = dot_tn(feed_rows, grad_uppre).astype(BF16)
-    result = hidden + scattered(dot_nn(after(inner, term_gate, term_up), w_down).astype(BF16), ring)
+    term_gate = dot_tn(feed_in, grad_gatepre).astype(BF16)
+    term_up = dot_tn(feed_in, grad_uppre).astype(BF16)
+    result_terms = dot_nn(inner, w_down).astype(BF16)
+    result = hidden + scattered(result_terms, ring)
     layer_output = result.astype(BF16).reshape(1, rows, width)
     down_share = lax.psum_scatter(term_down, "batch", scatter_dimension=0, tiled=True)
     term_feedpre = jnp.stack([term_gate, term_up]).reshape(2, ring, lines, own, hidden_part)
     term_feedpre = term_feedpre.transpose(2, 0, 1, 3, 4).reshape(-1, hidden_part)
+    feed_sum_start = term_feedpre
     feed_sum = lax.psum_scatter(
         after(term_feedpre, down_share), "batch", scatter_dimension=0, tiled=True
     )
@@ -834,19 +994,45 @@
     feed_share = exchanged(feed_share, mine, ring)
     gate_share = feed_share[:, 0].transpose(1, 0, 2).reshape(own, -1)
     up_share = feed_share[:, 1].transpose(1, 0, 2).reshape(own, -1)
-    term_feed = jnp.sum(grad_feedin * hidden * scale_two, axis=0)
-    scaled_two = grad_feedin * gain_two
-    grad_hidden = (
-        grad_own.astype(F32)
-        + scale_two * scaled_two
-        - hidden * scale_two**3 * jnp.mean(scaled_two * hidden, axis=-1, keepdims=True)
-    )
-
-    grad_branch = after(gathered(grad_hidden.astype(BF16), ring), term_gate, term_up)
+    if ring == 4:
+        grad_branch, grad_hidden, term_feed = fold(
+            finish_backward,
+            after(back_feedin, feed_sum_start).reshape(ring, rows, width),
+            (grad_own, hidden, gain_two[None]),
+            (
+                jax.ShapeDtypeStruct((rows, width), F32),
+                jax.ShapeDtypeStruct((1, width), F32),
+            ),
+            "fold_backward",
+        )
+        grad_branch, term_feed = grad_branch.reshape(length, width), term_feed[0]
+    else:
+        grad_feedin = scattered(back_feedin, ring)
+        scale_two = rms_scale(hidden)
+        term_feed = jnp.sum(grad_feedin * hidden * scale_two, axis=0)
+        scaled_two = grad_feedin * gain_two
+        grad_hidden = (
+            grad_own.astype(F32)
+            + scale_two * scaled_two
+            - hidden * scale_two**3 * jnp.mean(scaled_two * hidden, axis=-1, keepdims=True)
+        )
+        grad_branch = gathered(grad_hidden.astype(BF16), ring)
+
     grad_gated = whole_head(dot_nt(grad_branch, w_output))
     term_output = dot_tn(gated, grad_branch).astype(BF16)
+
+    def line_major(term):
+        return term.reshape(ring, lines, own, -1).transpose(1, 0, 2, 3).reshape(width, -1)
+
     slope = swish_sig * (1.0 + swish_pre * (1.0 - swish_sig))
     grad_swishpre = own_part((grad_gated * head_normed * slope).astype(BF16))
+    term_swish = line_major(dot_tn(normed, grad_swishpre).astype(BF16))
+    swish_sum = lax.psum_scatter(
+        after(term_swish, feed_sum), "batch", scatter_dimension=0, tiled=True
+    )
+    output_share = lax.psum_scatter(
+        after(term_output, swish_sum), "batch", scatter_dimension=0, tiled=True
+    )
     grad_normed_head = grad_gated * swish_act
     term_head = jnp.sum(grad_normed_head * head_plain, axis=0) / copies
     scaled_head = grad_normed_head * gain_head
@@ -873,22 +1059,23 @@
     term_expand = dot_nn(grad_logit, reduced) / copies
     grad_reduced = (dot_tn(grad_logit, expand_head) / copies).astype(BF16)
     grad_pre = jnp.concatenate(
-        [own_part(grad_query), own_part(grad_key), own_part(grad_value), grad_swishpre], axis=1
-    )
-    grad_normed = dot_nt(grad_pre, w_mixer) + dot_nn(grad_reduced, w_squeeze)
+        [own_part(grad_query), own_part(grad_key), own_part(grad_value)], axis=1
+    )
+    grad_normed = (
+        dot_nt(grad_pre, w_mixer) + dot_nt(grad_swishpre, w_swish) + dot_nn(grad_reduced, w_squeeze)
+    )
     term_mixer = (jnp.sum(grad_normed * plain_one, axis=0))
     term_squeeze = (dot_tn(grad_reduced, normed))
-    term_pre = dot_tn(normed, grad_pre).astype(BF16)
-    term_pre = term_pre.reshape(ring, lines, own, 4 * part).transpose(1, 0, 2, 3)
-    term_pre = term_pre.reshape(width, 4 * part)
-    grad_normed = (scattered(after(grad_normed.astype(BF16), term_pre), ring))
-    pre_share = lax.psum_scatter(after(term_pre, feed_sum), "batch", scatter_dimension=0, tiled=True)
-    output_share = lax.psum_scatter(
-        after(term_output, pre_share), "batch", scatter_dimension=0, tiled=True
-    )
-    pre_share = exchanged(pre_share.reshape(ring, own, 4 * part), mine, ring)
-    pre_share = pre_share.reshape(ring, own, 4, part).transpose(2, 1, 0, 3).reshape(4, own, width)
+    term_pre = line_major(dot_tn(normed, grad_pre).astype(BF16))
+    grad_normed = scattered(after(grad_normed.astype(BF16), term_pre), ring)
+    pre_sum = lax.psum_scatter(
+        after(term_pre, output_share), "batch", scatter_dimension=0, tiled=True
+    )
+    pre_share = exchanged(pre_sum.reshape(ring, own, 3 * part), mine, ring)
+    pre_share = pre_share.reshape(ring, own, 3, part).transpose(2, 1, 0, 3).reshape(3, own, width)
     pre_share = pre_share.astype(F32)
+    swish_share = exchanged(swish_sum.reshape(ring, own, part), mine, ring)
+    swish_share = swish_share.transpose(1, 0, 2).reshape(own, width).astype(F32)
     inputs_own = input_own.astype(F32)
     scale_own = rms_scale(inputs_own)
     scaled_one = grad_normed * (gain_one)
@@ -928,7 +1115,7 @@
         squeeze_share.reshape(own, RANK),
         expand_share.reshape(-1, RANK).T,
         bias_share,
-        pre_share[3],
+        swish_share,
         head_share,
         output_share.astype(F32),
         feedgain_share,

time: 711 us -> 815 us (1.15)
  Pallas kernels: 149 us -> 291 us
  starting transfers between devices: 50.9 us -> 24.7 us
  other arithmetic: 47.8 us -> 25.3 us
    pallas_call x1 -> x3, Pallas kernels: 117 us -> 259 us  [the longest x2 150 us: fold(): pl.pallas_call(functools.partial(fold_kernel, finish, len(given)), out_sh...]
    ppermute x34 -> x17, waiting for transfers between devices: 163 us -> 71.3 us  [swapped(): return lax.ppermute(block, 'seq', [(i, i ^ by) for i in range(ring)])]
    all_gather x2 -> x4, waiting for transfers between devices: 0.02 us -> 58 us  [the longest x2 29.2 us: over_batch(): lax.all_gather(blocks.reshape(-1, columns), 'batch', axis=0, tiled=False)]
    slice x11 -> x0, local copies, waits for them, and re-layouts: 20.1 us -> none  [the longest x3 13.7 us: local(): w_gate, w_up = (feed_blocks[0], feed_blocks[1])]
    reduce_scatter x2 -> x3, waiting for transfers between devices: 22 us -> 41.4 us  [the longest x1 30.1 us: local(): lax.psum_scatter(after(term_swish, feed_sum), 'batch', scatter_dimension=...]
    ppermute x34 -> x17, starting transfers between devices: 39 us -> 19.8 us  [swapped(): return lax.ppermute(block, 'seq', [(i, i ^ by) for i in range(ring)])]
    reduce_scatter x1, waiting for transfers between devices: 6.46 us -> 25.4 us  [local(): lax.psum_scatter(term_down, 'batch', scatter_dimension=0, tiled=True)]
    another operation x0 -> x4, local copies, waits for them, and re-layouts: none -> 16.5 us  [the longest x3 16.5 us: local(): w_gate, w_up = over_batch(after(feed_columns, w_output))]
  transfers between devices with their start and end apart: 45 -> 31, of which waited for: 30 -> 19; matrix products, arithmetic and copies ran while one was open for 39% -> 28% of each run, Pallas kernels for 5% -> 22%
where the time goes in v4:
time: 815 us; the launch traced here: 808 us
  Pallas kernels  291 us (36%)
  waiting for transfers between devices  199 us (24%)
  matrix products  158 us (19%)
  local copies, waits for them, and re-layouts  94 us (12%)
  other arithmetic  25.3 us (3%)
  starting transfers between devices  24.7 us (3%)
  between operations  15.5 us (2%)
    pallas_call x2, Pallas kernels, fold(): pl.pallas_call(functools.partial(fold_kernel, finish, len(given)), out_sh...  150 us
    pallas_call x1, Pallas kernels, start(): pl.pallas_call(functools.partial(start_kernel, ring, lines), out_shape=(g...  109 us
    ppermute x17, waiting for transfers between devices, swapped(): return lax.ppermute(block, 'seq', [(i, i ^ by) for i in range(ring)])  71.3 us
    dot_general x8, matrix products, dot_nt(): lax.dot_general(left, right, (((1,), (1,)), ((), ())), preferred_element_...  59.3 us
    dot_general x8, matrix products, dot_nn(): lax.dot_general(left, right, (((1,), (0,)), ((), ())), preferred_element_...  51 us
    dot_general x8, matrix products, dot_tn(): lax.dot_general(left, right, (((0,), (0,)), ((), ())), preferred_element_...  48 us
    unnamed x195, local copies, waits for them, and re-layouts  41.9 us
    reduce_scatter x1, waiting for transfers between devices, local(): lax.psum_scatter(after(term_swish, feed_sum), 'batch', scatter_dimension=...  30.1 us
  transfers between devices with their start and end apart: 31, of which 19 were waited for; matrix products, arithmetic and copies ran while one was open for 28% of the time, Pallas kernels for 22%

profile of v4, /device:TPU:0, one launch (start us, length us, event | category | flops | bytes accessed | tf_op | source)
XLA Modules:
  0.0 807.6 jit_solution(13188517527647680541)
XLA Ops:
  9.6 2.8 concatenate.49
  21.8 109.5 %start.1 = (bf16[4,256,2048]{2,1,0:T(8,128)(2,1)S(1)}, bf16[4,256,2048]{2,1,0:T(8,128)(2,1)S(1)}, bf16[4,8,64,1536]{3,2,1,0:T(8,128)(2,1)S(1)}, bf16[4,64,512]{2...) custom-call(bf16[256,2048]{1,0:T(8,128)(2,1)S(1)} %bitcast.203, ...), custom_call_target="tpu_custom_call" | custom-call | tf_op jit(solution)/shard_map/start/pallas_call | solution.py:582
  131.3 1.9 copy-done
  133.2 2.7 copy-done.44
  135.9 2.0 copy-done.45
  138.0 29.2 %all-gather.5.cloned.1.call-done = bf16[8,256,512]{2,1,0:T(8,128)(2,1)} async-done(((bf16[1,256,512]{2,1,0:T(8,128)(2,1)}), bf16[8,256,512]{2,1,0:T(8,128)(2,1)}) %all-gather.5.cloned.1.call-update) | async-done | bytes 2097168 | tf_op jit(solution)/shard_map/all_gather | solution.py:910
  167.2 3.2 copy.75
  170.5 28.7 %all-gather.7.cloned.1.call-done = bf16[512,2048]{1,0:T(8,128)(2,1)} async-done(((bf16[64,2048]{1,0:T(8,128)(2,1)}), bf16[512,2048]{1,0:T(8,128)(2,1)}) %all-gather.7.cloned.1.call-update) | async-done | bytes 2097168 | tf_op jit(solution)/shard_map/all_gather | solution.py:915
  201.1 3.3 multiply_reduce_fusion.1
  208.2 1.8 slice-done.1
  210.0 6.9 convolution_convert_fusion.4
  216.9 1.6 fusion.23
  227.4 11.1 %mixer_forward.1 = (f32[1024,512]{1,0:T(8,128)S(1)}, f32[64,1024]{1,0:T(8,128)S(1)}, f32[64,1024]{1,0:T(8,128)S(1)}, f32[8,64,512]{2,1,0:T(8,128)S(1)}, f32[8,64,512]{2,1,0:T(8,128)S(1)}) custom-call(s32[1]{0:T(128)} %bitcast.mine, bf16[1024,512]{1,0:T(8,128)(2,1)S(1)} %copy-done.11, bf16[1024,512]{1,0:T(8,128)(2,1)S(1)} %copy-done.9, ...), custom_call_target="tpu_custom_call" | custom-call | flops 1048576000 | bytes 6291456 | tf_op jit(solution)/shard_map/mixer_forward/pallas_call | solution.py:311
  239.8 3.9 multiply_convert_fusion.6
  243.8 2.3 convolution_convert_fusion.6
  246.1 75.3 %fold_forward.1 = (bf16[4,256,2048]{2,1,0:T(8,128)(2,1)S(1)}, f32[256,2048]{1,0:T(8,128)S(1)}) custom-call(bf16[4,256,2048]{2,1,0:T(8,128)(2,1)S(1)} %bitcast.205, bf16[256,2048]{1,0:T(8,128)(2,1)S(1)} %bitcast.204, f32[1,2048]{1,0:T(1,128)S(1)} %reshape.447.refs_2_.refs_3_), custom_call_target="tpu_custom_call" | custom-call | tf_op jit(solution)/shard_map/fold_forward/pallas_call | solution.py:716
  322.8 2.0 copy-done.48
  324.8 9.9 %fusion.20 = (bf16[1,4,8,64,1408]{4,3,1,0,2:T(8,128)(2,1)}, bf16[1,4,8,64,1408]{4,3,1,0,2:T(8,128)(2,1)}) fusion(bf16[2,4,8,64,1408]{4,3,1,0,2:T(8,128)(2,1)} %bitcast.232), kind=kLoop, calls=%fused_computation.147 | loop fusion | bytes 23068672 | tf_op jit(solution)/shard_map/unstack | solution.py:916
  334.7 3.3 copy.76
  339.6 3.3 copy.77
  344.3 8.4 %fusion.25 = f32[1024,1408]{1,0:T(8,128)} fusion(bf16[1024,2048]{1,0:T(8,128)(2,1)S(1)} %bitcast.221, bf16[2048,1408]{1,0:T(8,128)(2,1)S(1)} %bitcast.236), kind=kOutput, calls=%fused_computation.152 | convolution fusion | flops 5905580032 | bytes 15728640 | tf_op jit(solution)/shard_map/dot_general | solution.py:25
  352.7 10.7 %multiply_convert_fusion.4 = (bf16[1024,1408]{1,0:T(8,128)(2,1)S(1)}, f32[1024,1408]{1,0:T(8,128)}) fusion(f32[1024,1408]{1,0:T(8,128)} %fusion.25, bf16[1024,2048]{1,0:T(8,128)(2,1)S(1)} %bitcast.222, bf16[2048,1408]{1,0:T(8,128)(2,1)S(1)} %bitcast.239), kind=kOutput, calls=%fused_computation.14 | convolution fusion | flops 5914230784 | bytes 24379392 | tf_op jit(solution)/shard_map/dot_general | solution.py:25
  363.4 1.6 copy-done.82
  365.0 8.1 %convolution_convert_fusion.3 = bf16[1408,2048]{1,0:T(8,128)(2,1)} fusion(bf16[1024,1408]{1,0:T(8,128)(2,1)S(1)} %get-tuple-element.207, bf16[1024,2048]{1,0:T(8,128)(2,1)S(1)} %bitcast.218), kind=kOutput, calls=%fused_computation.11 | convolution fusion | flops 5908463616 | bytes 12845056 | tf_op jit(solution)/shard_map/dot_general | solution.py:33
  373.4 15.9 %multiply_convert_fusion.2 = (bf16[1024,1408]{1,0:T(8,128)(2,1)}, bf16[1024,1408]{1,0:T(8,128)(2,1)}) fusion(f32[1024,1408]{1,0:T(8,128)} %fusion.25, f32[1024,1408]{1,0:T(8,128)} %get-tuple-element.208, bf16[1024,2048]{1,0:T(8,128)(2,1)} %bitcast.217, bf16[1408,2048]{1,0:T(8,128)(2,1)} %all-gather.11.cloned.1.call-done), kind=kOutput, calls=%fused_computation.12 | convolution fusion | flops 5924323328 | bytes 27262976 | tf_op jit(solution)/shard_map/dot_general | solution.py:29
  389.3 9.0 %convolution_convert_fusion.1 = bf16[2048,1408]{1,0:T(8,128)(2,1)S(1)} fusion(bf16[1024,2048]{1,0:T(8,128)(2,1)S(1)} %bitcast.223, bf16[1024,1408]{1,0:T(8,128)(2,1)} %get-tuple-element.132), kind=kOutput, calls=%fused_computation.9 | convolution fusion | flops 5908463616 | bytes 12845056 | tf_op jit(solution)/shard_map/dot_general | solution.py:33
  398.3 7.1 convolution_convert_fusion.2
  405.4 1.9 pad_maximum_fusion
  407.3 5.5 copy.93
  412.8 25.4 %reduce-scatter.6.cloned.1.call-done = bf16[176,2048]{1,0:T(8,128)(2,1)} async-done(((bf16[1408,2048]{1,0:T(8,128)(2,1)}), bf16[176,2048]{1,0:T(8,128)(2,1)}) %reduce-scatter.6.cloned.1.call-update) | async-done | bytes 720912 | tf_op jit(solution)/shard_map/reduce_scatter | solution.py:986
  438.3 11.7 %fusion.26 = f32[1024,2048]{1,0:T(8,128)} fusion(bf16[1024,1408]{1,0:T(8,128)(2,1)} %get-tuple-element.133, bf16[2048,1408]{1,0:T(8,128)(2,1)} %bitcast.237), kind=kOutput, calls=%fused_computation.153 | convolution fusion | flops 5905580032 | bytes 17039360 | tf_op jit(solution)/shard_map/dot_general | solution.py:29
  450.1 10.9 %add_convert_fusion = bf16[1024,2048]{1,0:T(8,128)(2,1)S(1)} fusion(f32[1024,2048]{1,0:T(8,128)} %fusion.26, bf16[1024,1408]{1,0:T(8,128)(2,1)S(1)} %copy-done.84, bf16[2048,1408]{1,0:T(8,128)(2,1)} %bitcast.238), kind=kOutput, calls=%fused_computation.5 | convolution fusion | flops 5909774336 | bytes 21233664 | tf_op jit(solution)/shard_map/dot_general | solution.py:29
  461.0 74.3 %fold_backward.1 = (bf16[4,256,2048]{2,1,0:T(8,128)(2,1)S(1)}, f32[256,2048]{1,0:T(8,128)S(1)}, f32[1,2048]{1,0:T(1,128)S(1)}) custom-call(bf16[4,256,2048]{2,1,0:T(8,128)(2,1)S(1)} %bitcast.206, bf16[256,2048]{1,0:T(8,128)(2,1)S(1)} %bitcast.208, f32[256,2048]{1,0:T(8,128)S(1)} %copy-done.7, f32[1,2048]{1,0:T(1,128)S(1)} %reshape.447.refs_2_.refs_3_), custom_call_target="tpu_custom_call" | custom-call | tf_op jit(solution)/shard_map/fold_backward/pallas_call | solution.py:716
  535.4 3.6 multiply_reduce_fusion.2
  542.0 20.4 %mixer_backward.1 = (bf16[1024,512]{1,0:T(8,128)(2,1)S(1)}, bf16[1024,512]{1,0:T(8,128)(2,1)S(1)}, bf16[1024,512]{1,0:T(8,128)(2,1)S(1)}, f32[64,1024]{1,0:T(8,128)S(1)}) custom-call(s32[1]{0:T(128)} %bitcast.mine, bf16[1024,512]{1,0:T(8,128)(2,1)S(1)} %copy-done.12, bf16[1024,512]{1,0:T(8,128)(2,1)S(1)} %copy-done.10, ...), custom_call_target="tpu_custom_call" | custom-call | flops 2097152000 | bytes 10485760 | tf_op jit(solution)/shard_map/mixer_backward/pallas_call | solution.py:346
  563.6 2.2 convolution_convert_fusion.9
  565.8 5.6 fusion.28
  571.5 9.1 %fusion.27 = f32[1024,2048]{1,0:T(8,128)} fusion(bf16[1024,1536]{1,0:T(8,128)(2,1)S(1)} %constant_dynamic-update-slice_fusion, bf16[2048,1536]{1,0:T(8,128)(2,1)S(1)} %bitcast.216), kind=kOutput, calls=%fused_computation.154 | convolution fusion | flops 6442450944 | bytes 17825792 | tf_op jit(solution)/shard_map/dot_general | solution.py:29
  580.6 8.8 %multiply_reduce_fusion = (f32[2048]{0:T(1024)S(1)}, bf16[1024,2048]{1,0:T(8,128)(2,1)}, bf16[1024,2048]{1,0:T(8,128)(2,1)S(1)}) fusion(bf16[4,256,2048]{2,1,0:T(8,128)(2,1)S(1)} %copy-done.2, f32[1024]{0:T(1024)S(1)} %bitcast.275, f32[2048]{0:T(1024)S(1)} %copy-done.73, bf16[1024,16]{0,1:T(8,128)(2,1)S(1)} %convolution_convert_fusion.9, ...), kind=kOutput, calls=%fused_computation.2 | convolution fusion | flops 85981184 | bytes 29478912 | tf_op jit(solution)/shard_map/dot_general | solution.py:25
  589.4 2.4 convolution_convert_fusion.7
  593.5 5.9 convolution_convert_fusion.8
  599.4 30.1 %reduce-scatter.10.cloned.1.call-done = bf16[256,512]{1,0:T(8,128)(2,1)} async-done(((bf16[2048,512]{1,0:T(8,128)(2,1)}), bf16[256,512]{1,0:T(8,128)(2,1)}) %reduce-scatter.10.cloned.1.call-update) | async-done | bytes 262160 | tf_op jit(solution)/shard_map/reduce_scatter | solution.py:1030
  631.4 3.5 fusion.29
  637.2 3.1 collective-permute-done.8
  641.8 9.8 %convolution_convert_fusion = bf16[2048,1536]{1,0:T(8,128)(2,1)S(1)} fusion(bf16[1024,2048]{1,0:T(8,128)(2,1)} %copy-done.55, bf16[1024,1536]{1,0:T(8,128)(2,1)} %copy-done.66), kind=kOutput, calls=%fused_computation.8 | convolution fusion | flops 6445596672 | bytes 13631488 | tf_op jit(solution)/shard_map/dot_general | solution.py:33
  651.6 3.3 copy.81
  654.9 11.3 %reduce-scatter.12.cloned.1.call-done = bf16[64,2048]{1,0:T(8,128)(2,1)} async-done(((bf16[512,2048]{1,0:T(8,128)(2,1)}), bf16[64,2048]{1,0:T(8,128)(2,1)}) %reduce-scatter.12.cloned.1.call-update) | async-done | bytes 262160 | tf_op jit(solution)/shard_map/reduce_scatter | solution.py:1033
  666.3 9.8 %convolution_convert_fusion.5 = bf16[1024,2048]{1,0:T(8,128)(2,1)S(1)} fusion(bf16[1024,1408]{1,0:T(8,128)(2,1)} %copy-done.82, bf16[1408,2048]{1,0:T(8,128)(2,1)} %all-gather.11.cloned.1.call-done), kind=kOutput, calls=%fused_computation.18 | convolution fusion | flops 5907677184 | bytes 12845056 | tf_op jit(solution)/shard_map/dot_general | solution.py:25
  685.0 18.2 %collective-permute-done.4 = bf16[128,2048]{1,0:T(8,128)(2,1)S(1)} collective-permute-done((bf16[128,2048]{1,0:T(8,128)(2,1)S(1)}, bf16[128,2048]{1,0:T(8,128)(2,1)S(1)}, u32[]{:S(2)}, u32[]{:S(2)}) %collective-permute-start.4) | collective-permute-done | bytes 524320 | tf_op jit(solution)/shard_map/ppermute | solution.py:737
  703.2 1.8 collective-permute-done.6
  707.9 1.7 collective-permute-start.5
  711.1 2.1 add_convert_fusion.5
  715.5 17.2 %collective-permute-done.7 = bf16[256,2048]{1,0:T(8,128)(2,1)S(1)} collective-permute-done((bf16[256,2048]{1,0:T(8,128)(2,1)}, bf16[256,2048]{1,0:T(8,128)(2,1)S(1)}, u32[]{:S(2)}, u32[]{:S(2)}) %collective-permute-start.7) | collective-permute-done | bytes 1048608 | tf_op jit(solution)/shard_map/ppermute | solution.py:737
  735.0 1.9 fusion.9
  737.0 2.5 collective-permute-start.21
  740.6 14.6 %collective-permute-done.3 = bf16[256,2048]{1,0:T(8,128)(2,1)S(1)} collective-permute-done((bf16[256,2048]{1,0:T(8,128)(2,1)S(1)}, bf16[256,2048]{1,0:T(8,128)(2,1)S(1)}, u32[]{:S(2)}, u32[]{:S(2)}) %collective-permute-start.3) | collective-permute-done | bytes 1048608 | tf_op jit(solution)/shard_map/ppermute | solution.py:737
  756.6 2.9 fusion.8
  760.8 4.7 collective-permute-done.21
  765.5 4.6 collective-permute-done.20
  772.6 2.5 collective-permute-start.18
  781.2 1.6 collective-permute-start.15
  786.5 2.8 collective-permute-done.15
  789.3 2.0 collective-permute-done.14
  792.7 2.8 reshape.452
  (348 shorter events, 84.2 us)
Async XLA Ops:
  7.2 160.0 %all-gather.5.cloned.1.call-start = ((), (), s32[]{:S(2)}) async-start(), calls=%async_computation.5 | async-start | bytes 2359296 | tf_op jit(solution)/shard_map/all_gather | solution.py:910
  137.9 61.3 %all-gather.7.cloned.1.call-start = ((), (), s32[]{:S(2)}) async-start(), calls=%async_computation.6 | async-start | bytes 2359296 | tf_op jit(solution)/shard_map/all_gather | solution.py:915
  170.5 154.3 %all-gather.9.cloned.1.call-start = ((), (), s32[]{:S(2)}) async-start(), calls=%async_computation.7 | async-start | bytes 12976128 | tf_op jit(solution)/shard_map/all_gather | solution.py:910
  199.2 174.1 %all-gather.11.cloned.1.call-start = ((), (), s32[]{:S(2)}) async-start(), calls=%async_computation.8 | async-start | bytes 6488064 | tf_op jit(solution)/shard_map/all_gather | solution.py:917
  199.8 5.8 copy-start.72
  200.3 5.3 copy-start.58
  200.4 6.4 copy-start.74
  218.5 219.7 %reduce-scatter.6.cloned.1.call-start = ((), (), s32[]{:S(2)}) async-start(), calls=%async_computation.9 | async-start | bytes 6488064 | tf_op jit(solution)/shard_map/reduce_scatter | solution.py:986
  227.4 12.3 %copy-start.52 = (bf16[4,256,2048]{2,1,0:T(8,128)(2,1)S(1)}, bf16[4,256,2048]{2,1,0:T(8,128)(2,1)}, u32[]{:S(2)}) copy-start(bf16[4,256,2048]{2,1,0:T(8,128)(2,1)} %copy-done.51) | copy-start | bytes 12582916
  227.4 12.3 %copy-start.62 = (bf16[1,4,8,64,512]{4,3,2,1,0:T(8,128)(2,1)S(1)}, bf16[1,4,8,64,512]{4,3,2,1,0:T(8,128)(2,1)}, u32[]{:S(2)}) copy-start(bf16[1,4,8,64,512]{4,3,2,1,0:T(8,128)(2,1)} %copy.75) | copy-start | bytes 6291460
  238.5 5.2 copy-start.19
  238.5 5.2 copy-start.21
  344.3 8.4 %copy-start.57 = (bf16[1,4,8,64,1408]{4,3,2,1,0:T(8,128)(2,1)S(1)}, bf16[1,4,8,64,1408]{4,3,2,1,0:T(8,128)(2,1)}, u32[]{:S(2)}) copy-start(bf16[1,4,8,64,1408]{4,3,2,1,0:T(8,128)(2,1)} %copy.77) | copy-start | bytes 17301508
  352.7 12.3 %copy-start.46 = (bf16[4,256,2048]{2,1,0:T(8,128)(2,1)S(1)}, bf16[4,256,2048]{2,1,0:T(8,128)(2,1)}, u32[]{:S(2)}) copy-start(bf16[4,256,2048]{2,1,0:T(8,128)(2,1)} %copy-done.45) | copy-start | bytes 12582916
  373.1 220.3 %reduce-scatter.8.cloned.1.call-start = ((), (), s32[]{:S(2)}) async-start(), calls=%async_computation.10 | async-start | bytes 12976128 | tf_op jit(solution)/shard_map/reduce_scatter | solution.py:990
  373.4 16.0 %copy-start.50 = (bf16[4,256,2048]{2,1,0:T(8,128)(2,1)S(1)}, bf16[4,256,2048]{2,1,0:T(8,128)(2,1)}, u32[]{:S(2)}) copy-start(bf16[4,256,2048]{2,1,0:T(8,128)(2,1)} %copy-done.48) | copy-start | bytes 12582916
  389.3 9.0 %copy-start.83 = (bf16[1024,1408]{1,0:T(8,128)(2,1)S(1)}, bf16[1024,1408]{1,0:T(8,128)(2,1)}, u32[]{:S(2)}) copy-start(bf16[1024,1408]{1,0:T(8,128)(2,1)} %get-tuple-element.133) | copy-start | bytes 8650756
  438.3 191.2 %reduce-scatter.10.cloned.1.call-start = ((), (), s32[]{:S(2)}) async-start(), calls=%async_computation.11 | async-start | bytes 2359296 | tf_op jit(solution)/shard_map/reduce_scatter | solution.py:1030
  438.3 11.8 %copy-start.84 = (bf16[1024,1408]{1,0:T(8,128)(2,1)S(1)}, bf16[1024,1408]{1,0:T(8,128)(2,1)}, u32[]{:S(2)}) copy-start(bf16[1024,1408]{1,0:T(8,128)(2,1)} %get-tuple-element.132) | copy-start | bytes 8650756
  450.1 10.9 %copy-start.7 = (f32[256,2048]{1,0:T(8,128)S(1)}, f32[256,2048]{1,0:T(8,128)}, u32[]{:S(2)}) copy-start(f32[256,2048]{1,0:T(8,128)} %copy-done.6) | copy-start | bytes 6291460
  450.1 10.9 %copy-start.14 = (bf16[1,256,2048]{2,1,0:T(8,128)(2,1)S(1)}, bf16[1,256,2048]{2,1,0:T(8,128)(2,1)}, u32[]{:S(2)}) copy-start(bf16[1,256,2048]{2,1,0:T(8,128)(2,1)} %param.40) | copy-start | bytes 3145732
  461.0 74.4 %copy-start.61 = (f32[1024,512]{1,0:T(8,128)S(1)}, f32[1024,512]{1,0:T(8,128)}, u32[]{:S(2)}) copy-start(f32[1024,512]{1,0:T(8,128)} %get-tuple-element.206) | copy-start | bytes 6291460
  461.0 74.4 %copy-start.77 = (bf16[512,2048]{1,0:T(8,128)(2,1)S(1)}, bf16[512,2048]{1,0:T(8,128)(2,1)}, u32[]{:S(2)}) copy-start(bf16[512,2048]{1,0:T(8,128)(2,1)} %all-gather.7.cloned.1.call-done) | copy-start | bytes 6291460
  539.0 26.8 %copy-start.78 = (bf16[1024,512]{1,0:T(8,128)(2,1)}, bf16[1024,512]{1,0:T(8,128)(2,1)S(1)}, u32[]{:S(2)}) copy-start(bf16[1024,512]{1,0:T(8,128)(2,1)S(1)} %get-tuple-element.138) | copy-start | bytes 3145732
  562.4 9.0 %slice-start.2 = ((s8[6291456]{0:T(1024)(128)(4,1)}), s8[4194304]{0:T(1024)(128)(4,1)S(1)}, s32[]{:S(2)}) async-start(s8[6291456]{0:T(1024)(128)(4,1)} %bitcast.214), calls=%async_computation.16 | async-start | bytes 8388608
  562.7 8.7 %copy-start.66 = (bf16[1024,1536]{1,0:T(8,128)(2,1)}, bf16[1024,1536]{1,0:T(8,128)(2,1)S(1)}, u32[]{:S(2)}) copy-start(bf16[1024,1536]{1,0:T(8,128)(2,1)S(1)} %constant_dynamic-update-slice_fusion) | copy-start | bytes 9437188
  565.8 5.6 slice-start.3
  571.4 9.2 %copy-start.2 = (bf16[4,256,2048]{2,1,0:T(8,128)(2,1)S(1)}, bf16[4,256,2048]{2,1,0:T(8,128)(2,1)}, u32[]{:S(2)}) copy-start(bf16[4,256,2048]{2,1,0:T(8,128)(2,1)} %copy-done) | copy-start | bytes 12582916
  571.4 9.2 %copy-start.59 = (bf16[2048,16]{1,0:T(8,128)(2,1)S(1)}, bf16[2048,16]{1,0:T(8,128)(2,1)}, u32[]{:S(2)}) copy-start(bf16[2048,16]{1,0:T(8,128)(2,1)} %copy-done.58) | copy-start | bytes 196612
  571.4 9.2 %copy-start.73 = (f32[2048]{0:T(1024)S(1)}, f32[2048]{0:T(1024)}, u32[]{:S(2)}) copy-start(f32[2048]{0:T(1024)} %copy-done.72) | copy-start | bytes 24580
  580.6 8.8 %copy-start.79 = (bf16[1024,512]{1,0:T(8,128)(2,1)S(1)}, bf16[1024,512]{1,0:T(8,128)(2,1)}, u32[]{:S(2)}) copy-start(bf16[1024,512]{1,0:T(8,128)(2,1)} %copy-done.78) | copy-start | bytes 3145732
  593.4 37.7 %copy-start.71 = (bf16[1024,16]{0,1:T(8,128)(2,1)S(1)}, bf16[1024,16]{0,1:T(8,128)(2,1)}, u32[]{:S(2)}) copy-start(bf16[1024,16]{0,1:T(8,128)(2,1)} %copy-done.70) | copy-start | bytes 98308
  593.4 72.8 %reduce-scatter.12.cloned.1.call-start = ((), (), s32[]{:S(2)}) async-start(), calls=%async_computation.12 | async-start | bytes 2359296 | tf_op jit(solution)/shard_map/reduce_scatter | solution.py:1033
  629.5 150.4 %reduce-scatter.14.cloned.1.call-start = ((), (), s32[]{:S(2)}) async-start(), calls=%async_computation.13 | async-start | bytes 7077888 | tf_op jit(solution)/shard_map/reduce_scatter | solution.py:1071
  635.7 4.6 collective-permute-start.8
  640.3 25.9 %collective-permute-start.9 = (f32[8,1352]{1,0:T(8,128)S(1)}, f32[8,1352]{1,0:T(8,128)S(1)}, u32[]{:S(2)}, u32[]{:S(2)}) collective-permute-start(f32[8,1352]{1,0:T(8,128)S(1)} %slice_select_fusion.1), channel_id=1, source_target_pairs={{0,8},{8,0},{16,24},{24,16},{1,9},{9,1},{17,25},{25,17},{2,10},{10... | collective-permute-start | bytes 129800 | tf_op jit(solution)/shard_map/ppermute | solution.py:769
  666.3 9.9 %collective-permute-start.10 = (f32[4,1352]{1,0:T(4,128)S(1)}, f32[4,1352]{1,0:T(4,128)S(1)}, u32[]{:S(2)}, u32[]{:S(2)}) collective-permute-start(f32[4,1352]{1,0:T(4,128)S(1)} %slice_select_fusion.2), channel_id=1, source_target_pairs={{0,4},{1,5},{2,6},{3,7},{4,0},{5,1},{6,2},{7,3},{8,12},{9,13},{10,... | collective-permute-start | bytes 64904 | tf_op jit(solution)/shard_map/ppermute | solution.py:769
  676.1 5.5 copy-start.60
  676.1 5.2 copy-start.53
  676.2 4.2 collective-permute-start.11
  677.4 33.7 %collective-permute-start = (bf16[128,2048]{1,0:T(8,128)(2,1)}, bf16[128,2048]{1,0:T(8,128)(2,1)}, u32[]{:S(2)}, u32[]{:S(2)}) collective-permute-start(bf16[128,2048]{1,0:T(8,128)(2,1)} %get-tuple-element.149), channel_id=1, source_target_pairs={{0,16},{8,24},{16,0},{24,8},{1,17},{9,25},{17,1},{25,9},{2,18},{10... | collective-permute-start | bytes 1572872 | tf_op jit(solution)/shard_map/ppermute | solution.py:737
  678.9 32.2 %collective-permute-start.2 = (bf16[128,2048]{1,0:T(8,128)(2,1)}, bf16[128,2048]{1,0:T(8,128)(2,1)}, u32[]{:S(2)}, u32[]{:S(2)}) collective-permute-start(bf16[128,2048]{1,0:T(8,128)(2,1)} %get-tuple-element.148), channel_id=1, source_target_pairs={{0,8},{8,0},{16,24},{24,16},{1,9},{9,1},{17,25},{25,17},{2,10},{10... | collective-permute-start | bytes 1572872 | tf_op jit(solution)/shard_map/ppermute | solution.py:737
  680.4 3.3 collective-permute-start.12
  681.6 21.6 %collective-permute-start.4 = (bf16[128,2048]{1,0:T(8,128)(2,1)S(1)}, bf16[128,2048]{1,0:T(8,128)(2,1)S(1)}, u32[]{:S(2)}, u32[]{:S(2)}) collective-permute-start(bf16[128,2048]{1,0:T(8,128)(2,1)S(1)} %get-tuple-element.143), channel_id=1, source_target_pairs={{0,16},{8,24},{16,0},{24,8},{1,17},{9,25},{17,1},{25,9},{2,18},{10... | collective-permute-start | bytes 1572872 | tf_op jit(solution)/shard_map/ppermute | solution.py:737
  682.2 22.8 %collective-permute-start.6 = (bf16[128,2048]{1,0:T(8,128)(2,1)S(1)}, bf16[128,2048]{1,0:T(8,128)(2,1)S(1)}, u32[]{:S(2)}, u32[]{:S(2)}) collective-permute-start(bf16[128,2048]{1,0:T(8,128)(2,1)S(1)} %get-tuple-element.142), channel_id=1, source_target_pairs={{0,8},{8,0},{16,24},{24,16},{1,9},{9,1},{17,25},{25,17},{2,10},{10... | collective-permute-start | bytes 1572872 | tf_op jit(solution)/shard_map/ppermute | solution.py:737
  706.5 26.2 %collective-permute-start.7 = (bf16[256,2048]{1,0:T(8,128)(2,1)}, bf16[256,2048]{1,0:T(8,128)(2,1)S(1)}, u32[]{:S(2)}, u32[]{:S(2)}) collective-permute-start(bf16[256,2048]{1,0:T(8,128)(2,1)} %pad_maximum_fusion.6), channel_id=1, source_target_pairs={{0,16},{8,24},{16,0},{24,8},{1,17},{9,25},{17,1},{25,9},{2,18},{10... | collective-permute-start | bytes 3145736 | tf_op jit(solution)/shard_map/ppermute | solution.py:737
  707.9 26.2 %collective-permute-start.5 = (bf16[256,2048]{1,0:T(8,128)(2,1)}, bf16[256,2048]{1,0:T(8,128)(2,1)S(1)}, u32[]{:S(2)}, u32[]{:S(2)}) collective-permute-start(bf16[256,2048]{1,0:T(8,128)(2,1)} %pad_maximum_fusion.5), channel_id=1, source_target_pairs={{0,8},{8,0},{16,24},{24,16},{1,9},{9,1},{17,25},{25,17},{2,10},{10... | collective-permute-start | bytes 3145736 | tf_op jit(solution)/shard_map/ppermute | solution.py:737
  711.1 23.0 %copy-start.5 = (bf16[1,256,2048]{2,1,0:T(8,128)(2,1)S(1)}, bf16[1,256,2048]{2,1,0:T(8,128)(2,1)}, u32[]{:S(2)}) copy-start(bf16[1,256,2048]{2,1,0:T(8,128)(2,1)} %param.24) | copy-start | bytes 3145732
  711.1 23.0 %copy-start.54 = (bf16[1024,2048]{1,0:T(8,128)(2,1)S(1)}, bf16[1024,2048]{1,0:T(8,128)(2,1)}, u32[]{:S(2)}) copy-start(bf16[1024,2048]{1,0:T(8,128)(2,1)} %get-tuple-element.72) | copy-start | bytes 12582916
  713.3 41.8 %collective-permute-start.3 = (bf16[256,2048]{1,0:T(8,128)(2,1)S(1)}, bf16[256,2048]{1,0:T(8,128)(2,1)S(1)}, u32[]{:S(2)}, u32[]{:S(2)}) collective-permute-start(bf16[256,2048]{1,0:T(8,128)(2,1)S(1)} %pad_maximum_fusion.4), channel_id=1, source_target_pairs={{0,16},{8,24},{16,0},{24,8},{1,17},{9,25},{17,1},{25,9},{2,18},{10... | collective-permute-start | bytes 3145736 | tf_op jit(solution)/shard_map/ppermute | solution.py:737
  714.7 20.3 %copy-start.16 = (f32[256,2048]{1,0:T(8,128)S(1)}, f32[256,2048]{1,0:T(8,128)}, u32[]{:S(2)}) copy-start(f32[256,2048]{1,0:T(8,128)} %copy-done.15) | copy-start | bytes 6291460
  714.8 41.8 %collective-permute-start.1 = (bf16[256,2048]{1,0:T(8,128)(2,1)S(1)}, bf16[256,2048]{1,0:T(8,128)(2,1)S(1)}, u32[]{:S(2)}, u32[]{:S(2)}) collective-permute-start(bf16[256,2048]{1,0:T(8,128)(2,1)S(1)} %pad_maximum_fusion.3), channel_id=1, source_target_pairs={{0,8},{8,0},{16,24},{24,16},{1,9},{9,1},{17,25},{25,17},{2,10},{10... | collective-permute-start | bytes 3145736 | tf_op jit(solution)/shard_map/ppermute | solution.py:737
  736.9 19.7 %copy-start.8 = (f32[256,2048]{1,0:T(8,128)S(1)}, f32[256,2048]{1,0:T(8,128)}, u32[]{:S(2)}) copy-start(f32[256,2048]{1,0:T(8,128)} %copy-done.6) | copy-start | bytes 6291460
  737.0 28.5 %collective-permute-start.21 = (bf16[2,64,1408]{2,1,0:T(8,128)(2,1)S(1)}, bf16[2,64,1408]{2,1,0:T(8,128)(2,1)S(1)}, u32[]{:S(2)}, u32[]{:S(2)}) collective-permute-start(bf16[2,64,1408]{2,1,0:T(8,128)(2,1)S(1)} %get-tuple-element.165), channel_id=1, source_target_pairs={{0,24},{8,16},{16,8},{24,0},{1,25},{9,17},{17,9},{25,1},{2,26},{10... | collective-permute-start | bytes 1081352 | tf_op jit(solution)/shard_map/ppermute | solution.py:737
  739.5 30.5 %collective-permute-start.20 = (bf16[2,64,1408]{2,1,0:T(8,128)(2,1)S(1)}, bf16[2,64,1408]{2,1,0:T(8,128)(2,1)S(1)}, u32[]{:S(2)}, u32[]{:S(2)}) collective-permute-start(bf16[2,64,1408]{2,1,0:T(8,128)(2,1)S(1)} %get-tuple-element.166), channel_id=1, source_target_pairs={{0,16},{8,24},{16,0},{24,8},{1,17},{9,25},{17,1},{25,9},{2,18},{10... | collective-permute-start | bytes 1081352 | tf_op jit(solution)/shard_map/ppermute | solution.py:737
  740.2 19.3 %copy-start.65 = (bf16[176,2048]{1,0:T(8,128)(2,1)S(1)}, bf16[176,2048]{1,0:T(8,128)(2,1)}, u32[]{:S(2)}) copy-start(bf16[176,2048]{1,0:T(8,128)(2,1)} %reduce-scatter.6.cloned.1.call-done) | copy-start | bytes 2162692
  740.2 31.2 %collective-permute-start.19 = (bf16[2,64,1408]{2,1,0:T(8,128)(2,1)S(1)}, bf16[2,64,1408]{2,1,0:T(8,128)(2,1)S(1)}, u32[]{:S(2)}, u32[]{:S(2)}) collective-permute-start(bf16[2,64,1408]{2,1,0:T(8,128)(2,1)S(1)} %get-tuple-element.167), channel_id=1, source_target_pairs={{0,8},{8,0},{16,24},{24,16},{1,9},{9,1},{17,25},{25,17},{2,10},{10... | collective-permute-start | bytes 1081352 | tf_op jit(solution)/shard_map/ppermute | solution.py:737
  772.6 6.2 collective-permute-start.18
  775.0 4.3 collective-permute-start.17
  775.5 4.3 collective-permute-start.16
  777.6 8.0 copy-start.67
  781.2 8.1 %collective-permute-start.15 = (bf16[64,1536]{1,0:T(8,128)(2,1)S(1)}, bf16[64,1536]{1,0:T(8,128)(2,1)S(1)}, u32[]{:S(2)}, u32[]{:S(2)}) collective-permute-start(bf16[64,1536]{1,0:T(8,128)(2,1)S(1)} %get-tuple-element.173), channel_id=1, source_target_pairs={{0,24},{8,16},{16,8},{24,0},{1,25},{9,17},{17,9},{25,1},{2,26},{10... | collective-permute-start | bytes 589832 | tf_op jit(solution)/shard_map/ppermute | solution.py:737
  782.8 8.5 %collective-permute-start.14 = (bf16[64,1536]{1,0:T(8,128)(2,1)S(1)}, bf16[64,1536]{1,0:T(8,128)(2,1)S(1)}, u32[]{:S(2)}, u32[]{:S(2)}) collective-permute-start(bf16[64,1536]{1,0:T(8,128)(2,1)S(1)} %get-tuple-element.174), channel_id=1, source_target_pairs={{0,16},{8,24},{16,0},{24,8},{1,17},{9,25},{17,1},{25,9},{2,18},{10... | collective-permute-start | bytes 589832 | tf_op jit(solution)/shard_map/ppermute | solution.py:737
  783.3 8.0 collective-permute-start.13
  (58 other events, 137.6 us)
Sparse Core Ops, SparseCore 0:
  138.0 29.1 all-gather.4
  170.6 28.5 all-gather.6
  200.9 107.5 all-gather.8
  309.9 58.7 all-gather.10
  373.2 64.9 reduce-scatter.5
  440.4 117.6 reduce-scatter.7
  593.6 35.8 reduce-scatter.9
  631.7 34.4 reduce-scatter.11
  668.5 68.7 reduce-scatter.13

commit v5 on v4

--- a/solution.py
+++ b/solution.py
@@ -463,8 +463,8 @@
 
 
 def start_kernel(
-    ring, lines, inputs, cotangent, w_query, w_key, w_value, w_swish, w_out, gate, up, small,
-    inputs_all, cotangent_all, w_mixer, swish_columns, out_rows, feed_columns, small_all,
+    ring, lines, inputs, w_query, w_key, w_value, w_swish, w_out, gate, up, small,
+    inputs_all, w_mixer, swish_columns, out_rows, feed_columns, small_all,
     local_sem, send_sem, recv_sem,
 ):
     mine, batch = lax.axis_index("seq"), lax.axis_index("batch")
@@ -554,44 +554,40 @@
         for to in others
         for at, ref in enumerate((gate, up))
     ]
-    own_cotangent, cotangent_waits = sent(cotangent, cotangent_all)
     for step in range(1, chips + 1):
         for chain in chains:
             if chips > 1 or step > 1:
                 next(chain)
-        if step == min(2, chips):
-            cotangent_waits = passed_on(cotangent_all, cotangent_waits)
     if chips == 1:
         for chain in chains:
             next(chain)
-    for wait in input_waits + cotangent_waits + other_waits:
+    for wait in input_waits + other_waits:
         wait()
-    for copy in [own_input, own_cotangent] + own_columns:
+    for copy in [own_input] + own_columns:
         copy.wait()
     copies.close()
 
 
-def start(ring, lines, inputs, cotangent, columns, w_out, gate, up, small):
+def start(ring, lines, inputs, columns, w_out, gate, up, small):
     own, width = columns[0].shape
     part, hidden = width // ring, gate.shape[1] // ring
     if hidden % 128:
         gate, up = (a.reshape(own, ring, hidden).transpose(1, 0, 2) for a in (gate, up))
+    inside, anywhere = (pl.BlockSpec(memory_space=space) for space in (pltpu.VMEM, pl.ANY))
     chains = 2 * ring
-    away = (ring - 1) * 9 + 4 + chains * (4 * (lines // 2 - 1) + 1)
-    gathered_shape = jax.ShapeDtypeStruct((ring,) + inputs.shape, BF16)
+    away = (ring - 1) * 9 + 2 + chains * (4 * (lines // 2 - 1) + 1)
     return pl.pallas_call(
         functools.partial(start_kernel, ring, lines),
         out_shape=(
-            gathered_shape,
-            gathered_shape,
+            jax.ShapeDtypeStruct((ring,) + inputs.shape, BF16),
             jax.ShapeDtypeStruct((ring, lines, own, 3 * part), BF16),
             jax.ShapeDtypeStruct((ring, own, part), BF16),
             jax.ShapeDtypeStruct(w_out.shape, BF16),
             jax.ShapeDtypeStruct((2, ring, own, hidden), BF16),
             jax.ShapeDtypeStruct((ring, lines) + small.shape, BF16),
         ),
-        in_specs=[pl.BlockSpec(memory_space=pltpu.VMEM)] * 10,
-        out_specs=[pl.BlockSpec(memory_space=pl.ANY)] * 7,
+        in_specs=[inside] * 4 + [anywhere] * 4 + [inside],
+        out_specs=[anywhere] * 6,
         scratch_shapes=[
             pltpu.SemaphoreType.DMA((12,)),
             pltpu.SemaphoreType.DMA((away,)),
@@ -599,7 +595,7 @@
         ],
         compiler_params=pltpu.CompilerParams(has_side_effects=True, vmem_limit_bytes=32 << 20),
         name="start",
-    )(inputs, cotangent, *columns, w_out, gate, up, small)
+    )(inputs, *columns, w_out, gate, up, small)
 
 
 PARTS = 4
@@ -707,6 +703,261 @@
     )
     made[0][full, :] = grad
     return grad.astype(BF16)
+
+
+def finish_kernel(
+    lines, mixer_terms, out_terms, input_terms, feed_sum, small_terms, inputs, gain, grad_hidden,
+    grad_query, grad_key, grad_value, grad_swish, grad_out, grad_gate, grad_up, grad_input, small_sum,
+    crossed, staged, arrived, summed, outgoing, mixer_blocks, feed_blocks, small_ring, small_mine, small_line,
+    first, second, third, two_low, one_high, local_sem, send_sem, recv_sem,
+):
+    mine, batch = lax.axis_index("seq"), lax.axis_index("batch")
+    chips = lines // 2
+    chip, core = batch // 2, batch % 2
+    sibling = chip * 2 + (1 - core)
+    others = peers(4, mine)
+    row, col = (others[0], batch), (others[1], batch)
+    copies = Copies(local_sem, send_sem, recv_sem)
+    slabs = others + [mine, None]
+
+    def term(slab, owner):
+        return out_terms.at[owner] if slabs[slab] is None else mixer_terms.at[slabs[slab], owner]
+
+    cross_waits = {}
+    for slab in range(len(slabs)):
+        for owner in range(chips):
+            cross_waits[slab, owner] = copies.far(
+                term(slab, owner * 2 + (1 - core)),
+                crossed.at[slab, owner],
+                crossed.at[slab, owner],
+                (mine, sibling),
+            )
+    small_waits = [
+        copies.far(small_terms.at[to], small_ring.at[at], small_ring.at[at], (to, batch))
+        for at, to in enumerate(others)
+    ]
+    feed_waits = [
+        copies.far(feed_sum.at[:, to], feed_blocks.at[mine], feed_blocks.at[to], (to, batch))
+        for to in others
+    ]
+
+    size = input_terms.shape[1] // PARTS
+    opening, direct = [], []
+
+    def span(at):
+        low = pl.ds(at * size, size // 2)
+        return pl.ds(at * size, size), low, pl.ds(at * size + size // 2, size // 2)
+
+    def open_part(at):
+        _, low, high = span(at)
+        opening.append(
+            (
+                copies.far(input_terms.at[3, low], first.at[low], first.at[low], row),
+                copies.far(input_terms.at[3, high], first.at[high], first.at[high], col),
+            )
+        )
+
+    def pass_part(at):
+        _, low, high = span(at)
+        waits = [
+            copies.far(input_terms.at[2, high], second.at[high], second.at[high], col),
+            copies.far(input_terms.at[1, low], third.at[low], third.at[low], row),
+        ]
+        opening[at][0]()
+        two_low[low, :] = added(input_terms[2, low, :], first[low, :])
+        waits.append(copies.far(two_low.at[low], second.at[low], second.at[low], col))
+        opening[at][1]()
+        one_high[high, :] = added(input_terms[1, high, :], first[high, :])
+        waits.append(copies.far(one_high.at[high], third.at[high], third.at[high], row))
+        direct.append(waits)
+
+    def close_part(at):
+        full, _, _ = span(at)
+        for wait in direct[at]:
+            wait()
+        total = (
+            input_terms[0, full, :].astype(F32)
+            + second[full, :].astype(F32)
+            + third[full, :].astype(F32)
+        )
+        features = inputs[full, :].astype(F32)
+        scale = rms_scale(features)
+        plain = features * scale
+        scaled = total * gain[...]
+        grad = (
+            grad_hidden[full, :]
+            + scale * scaled
+            - plain * (scale * jnp.mean(scaled * plain, axis=-1, keepdims=True))
+        )
+        grad_input[full, :] = grad.astype(BF16)
+
+    def small_part():
+        for wait in small_waits:
+            wait()
+        small_mine[...] = small_terms[mine] + small_ring[0] + small_ring[1] + small_ring[2]
+        for by in range(1, lines):
+            to, source = (batch + by) % lines, (batch + lines - by) % lines
+            small_waits.append(
+                copies.far(small_mine.at[to], small_line.at[by], small_line.at[by], (mine, to))
+            )
+
+    def feed_part():
+        for wait in feed_waits:
+            wait()
+        feed_blocks[mine] = feed_sum[:, mine]
+        wide = feed_sum.shape[3]
+        for source in range(4):
+            at = pl.ds(source * wide, wide)
+            grad_gate[:, at] = feed_blocks[source, 0].astype(F32)
+            grad_up[:, at] = feed_blocks[source, 1].astype(F32)
+
+    beside = [functools.partial(open_part, 1)]
+    for at in range(PARTS):
+        if at + 2 <= PARTS - 1:
+            beside.append(functools.partial(open_part, at + 2))
+        beside.append(functools.partial(pass_part, at))
+        if at == 0:
+            beside.append(small_part)
+        if at:
+            beside.append(functools.partial(close_part, at - 1))
+    beside.append(functools.partial(close_part, PARTS - 1))
+    beside.append(feed_part)
+    open_part(0)
+
+    def both_cores(slab, owner):
+        return term(slab, owner * 2 + core)[...].astype(F32) + crossed[slab, owner].astype(F32)
+
+    crossed_in = set()
+
+    def wait_cross(slab):
+        if slab not in crossed_in:
+            crossed_in.add(slab)
+            for owner in range(chips):
+                cross_waits[slab, owner]()
+
+    flying = {}
+    for far in range(chips - 1, 0, -1):
+        for slab in range(len(slabs)):
+            wait_cross(slab)
+            for side, way in enumerate((1, -1)):
+                owner = chip + way * far
+                sends = (owner >= 0) & (owner < chips)
+                held = jnp.clip(owner, 0, chips - 1)
+                before = chip - way
+                gets = sends & (before >= 0) & (before < chips)
+                here = staged.at[side, far - 1, slab]
+                if far < chips - 1:
+                    wait = flying[side, far + 1, slab]
+
+                    @pl.when(gets)
+                    def _(wait=wait, slab=slab, held=held, here=here, side=side, far=far):
+                        wait()
+                        here[...] = (
+                            both_cores(slab, held) + arrived[side, far, slab].astype(F32)
+                        ).astype(BF16)
+
+                    @pl.when(sends & jnp.logical_not((before >= 0) & (before < chips)))
+                    def _(slab=slab, held=held, here=here):
+                        here[...] = both_cores(slab, held).astype(BF16)
+                else:
+
+                    @pl.when(sends)
+                    def _(slab=slab, held=held, here=here):
+                        here[...] = both_cores(slab, held).astype(BF16)
+
+                target = jnp.clip(chip + way, 0, chips - 1) * 2 + core
+                flying[side, far, slab] = copies.far(
+                    here,
+                    arrived.at[side, far - 1, slab],
+                    arrived.at[side, far - 1, slab],
+                    (mine, target),
+                    sends,
+                )
+            if beside:
+                beside.pop(0)()
+    ring_waits = []
+    for slab in range(len(slabs)):
+        total = summed.at[slab]
+        total[...] = both_cores(slab, chip)
+        for side, way in enumerate((1, -1)):
+            before = chip - way
+            wait = flying[side, 1, slab]
+
+            @pl.when((before >= 0) & (before < chips))
+            def _(wait=wait, total=total, slab=slab, side=side):
+                wait()
+                total[...] += arrived[side, 0, slab].astype(F32)
+
+        if slabs[slab] is None:
+            grad_out[...] = total[...]
+        elif slab == len(others):
+            mixer_blocks[mine] = total[...].astype(BF16)
+        else:
+            outgoing[slab] = total[...].astype(BF16)
+            to = slabs[slab]
+            ring_waits.append(
+                copies.far(
+                    outgoing.at[slab], mixer_blocks.at[mine], mixer_blocks.at[to], (to, batch)
+                )
+            )
+        if beside:
+            beside.pop(0)()
+    for piece in beside:
+        piece()
+    for wait in small_waits[3:]:
+        wait()
+    total = small_mine[batch]
+    for by in range(1, lines):
+        total = total + small_line[by]
+    small_sum[...] = total
+    for wait in ring_waits:
+        wait()
+    part = grad_query.shape[1] // 4
+    for source in range(4):
+        at = pl.ds(source * part, part)
+        for piece, out in enumerate((grad_query, grad_key, grad_value, grad_swish)):
+            out[:, at] = mixer_blocks[source, :, piece * part : (piece + 1) * part].astype(F32)
+    copies.close()
+
+
+def finish(lines, mixer_terms, out_terms, input_terms, feed_sum, small_terms, inputs, gain, grad_hidden):
+    ring, _, own, width = mixer_terms.shape
+    rows, hidden = inputs.shape[0], feed_sum.shape[3]
+    chips = lines // 2
+    inside = pl.BlockSpec(memory_space=pltpu.VMEM)
+    block = pltpu.VMEM((rows, width), BF16)
+    small = small_terms.shape[2:]
+    away = (ring + 1) * (chips + 2 * (chips - 1)) + 3 * (ring - 1) + PARTS * 6 + lines - 1
+    square = jax.ShapeDtypeStruct((own, width), F32)
+    wide = jax.ShapeDtypeStruct((own, ring * hidden), F32)
+    return pl.pallas_call(
+        functools.partial(finish_kernel, lines),
+        out_shape=(square,) * 5
+        + (wide,) * 2
+        + (jax.ShapeDtypeStruct((rows, width), BF16), jax.ShapeDtypeStruct(small, F32)),
+        in_specs=[inside] * 8,
+        out_specs=[inside] * 9,
+        scratch_shapes=[
+            pltpu.VMEM((ring + 1, chips, own, width), BF16),
+            pltpu.VMEM((2, chips - 1, ring + 1, own, width), BF16),
+            pltpu.VMEM((2, chips - 1, ring + 1, own, width), BF16),
+            pltpu.VMEM((ring + 1, own, width), F32),
+            pltpu.VMEM((ring - 1, own, width), BF16),
+            pltpu.VMEM((ring, own, width), BF16),
+            pltpu.VMEM((ring, 2, own, hidden), BF16),
+            pltpu.VMEM((ring - 1, lines) + small, F32),
+            pltpu.VMEM((lines,) + small, F32),
+            pltpu.VMEM((lines,) + small, F32),
+        ]
+        + [block] * 5
+        + [
+            pltpu.SemaphoreType.DMA((1,)),
+            pltpu.SemaphoreType.DMA((away,)),
+            pltpu.SemaphoreType.DMA((away,)),
+        ],
+        compiler_params=pltpu.CompilerParams(has_side_effects=True, vmem_limit_bytes=58 << 20),
+        name="finish",
+    )(mixer_terms, out_terms, input_terms, feed_sum, small_terms, inputs, gain, grad_hidden)
 
 
 def fold(finish, terms, given, made, name):
@@ -873,11 +1124,10 @@
     params = jnp.pad(params, (0, -params.shape[0] % 2048)).reshape(-1, 128)
     input_own = layer_input.reshape(rows, width)
     grad_own = cotangent.reshape(rows, width)
-    inputs, grad_out, w_mixer, swish_columns, out_rows, feed_columns, small = start(
+    inputs, w_mixer, swish_columns, out_rows, feed_columns, small = start(
         ring,
         lines,
         input_own,
-        grad_own,
         (query_weight, key_weight, value_weight, swish_weight),
         output_weight,
         gate_weight,
@@ -885,7 +1135,7 @@
         params,
     )
     inputs = inputs.reshape(length, width)
-    grad_out = grad_out.reshape(length, width)
+    grad_out = gathered(after(grad_own, inputs), ring)
     w_mixer = w_mixer.reshape(width, 3 * part)
     small = small.reshape(devices, -1)
     segment = lax.dynamic_index_in_dim(
@@ -912,9 +1162,9 @@
         return full.transpose(1, 2, 0, 3, 4).reshape(kinds, width, columns)
 
     w_swish = over_batch(swish_columns[None])[0]
-    w_output = lax.all_gather(after(out_rows, w_swish), "batch", axis=0, tiled=True)
-    w_gate, w_up = over_batch(after(feed_columns, w_output))
-    w_down = lax.all_gather(after(down_weight, w_output), "batch", axis=0, tiled=True)
+    w_output = lax.all_gather(out_rows, "batch", axis=0, tiled=True)
+    w_gate, w_up = over_batch(feed_columns)
+    w_down = lax.all_gather(after(down_weight, feed_columns), "batch", axis=0, tiled=True)
 
     chunked = segment.reshape(-1, CHUNK)
     before = jnp.concatenate([jnp.full((1,), -1.0, F32), chunked[:-1, -1]])
@@ -944,6 +1194,7 @@
     log_rate = jax.nn.log_sigmoid(forget_logit) / TAU_GATE
     inflow = -jnp.expm1(log_rate)
     order = mine.reshape(1).astype(jnp.int32)
+    query, grad_out = lax.optimization_barrier((query, grad_out))
     mixed, attention, logits, key_start, value_start = mixer_forward(
         order, ring, query, key, value, log_rate, inflow, mask_rows, segment_col
     )
@@ -978,26 +1229,22 @@
     grad_gatepre = grad_gatepre.astype(BF16)
     grad_uppre = (grad_inner * gate_act).astype(BF16)
     back_feedin = (dot_nt(grad_gatepre, w_gate) + dot_nt(grad_uppre, w_up)).astype(BF16)
-    term_gate = dot_tn(feed_in, grad_gatepre).astype(BF16)
-    term_up = dot_tn(feed_in, grad_uppre).astype(BF16)
+    feed_rows = after(feed_in, back_feedin)
+    term_gate = dot_tn(feed_rows, grad_gatepre).astype(BF16)
+    term_up = dot_tn(feed_rows, grad_uppre).astype(BF16)
     result_terms = dot_nn(inner, w_down).astype(BF16)
     result = hidden + scattered(result_terms, ring)
     layer_output = result.astype(BF16).reshape(1, rows, width)
     down_share = lax.psum_scatter(term_down, "batch", scatter_dimension=0, tiled=True)
     term_feedpre = jnp.stack([term_gate, term_up]).reshape(2, ring, lines, own, hidden_part)
     term_feedpre = term_feedpre.transpose(2, 0, 1, 3, 4).reshape(-1, hidden_part)
-    feed_sum_start = term_feedpre
     feed_sum = lax.psum_scatter(
         after(term_feedpre, down_share), "batch", scatter_dimension=0, tiled=True
     )
-    feed_share = feed_sum.reshape(2, ring, own, hidden_part).transpose(1, 0, 2, 3)
-    feed_share = exchanged(feed_share, mine, ring)
-    gate_share = feed_share[:, 0].transpose(1, 0, 2).reshape(own, -1)
-    up_share = feed_share[:, 1].transpose(1, 0, 2).reshape(own, -1)
     if ring == 4:
         grad_branch, grad_hidden, term_feed = fold(
             finish_backward,
-            after(back_feedin, feed_sum_start).reshape(ring, rows, width),
+            after(back_feedin, term_feedpre).reshape(ring, rows, width),
             (grad_own, hidden, gain_two[None]),
             (
                 jax.ShapeDtypeStruct((rows, width), F32),
@@ -1026,13 +1273,6 @@
 
     slope = swish_sig * (1.0 + swish_pre * (1.0 - swish_sig))
     grad_swishpre = own_part((grad_gated * head_normed * slope).astype(BF16))
-    term_swish = line_major(dot_tn(normed, grad_swishpre).astype(BF16))
-    swish_sum = lax.psum_scatter(
-        after(term_swish, feed_sum), "batch", scatter_dimension=0, tiled=True
-    )
-    output_share = lax.psum_scatter(
-        after(term_output, swish_sum), "batch", scatter_dimension=0, tiled=True
-    )
     grad_normed_head = grad_gated * swish_act
     term_head = jnp.sum(grad_normed_head * head_plain, axis=0) / copies
     scaled_head = grad_normed_head * gain_head
@@ -1064,28 +1304,9 @@
     grad_normed = (
         dot_nt(grad_pre, w_mixer) + dot_nt(grad_swishpre, w_swish) + dot_nn(grad_reduced, w_squeeze)
     )
+    term_pre = dot_tn(normed, jnp.concatenate([grad_pre, grad_swishpre], axis=1)).astype(BF16)
     term_mixer = (jnp.sum(grad_normed * plain_one, axis=0))
     term_squeeze = (dot_tn(grad_reduced, normed))
-    term_pre = line_major(dot_tn(normed, grad_pre).astype(BF16))
-    grad_normed = scattered(after(grad_normed.astype(BF16), term_pre), ring)
-    pre_sum = lax.psum_scatter(
-        after(term_pre, output_share), "batch", scatter_dimension=0, tiled=True
-    )
-    pre_share = exchanged(pre_sum.reshape(ring, own, 3 * part), mine, ring)
-    pre_share = pre_share.reshape(ring, own, 3, part).transpose(2, 1, 0, 3).reshape(3, own, width)
-    pre_share = pre_share.astype(F32)
-    swish_share = exchanged(swish_sum.reshape(ring, own, part), mine, ring)
-    swish_share = swish_share.transpose(1, 0, 2).reshape(own, width).astype(F32)
-    inputs_own = input_own.astype(F32)
-    scale_own = rms_scale(inputs_own)
-    scaled_one = grad_normed * (gain_one)
-    grad_inputs = (
-        grad_hidden
-        + scale_own * scaled_one
-        - inputs_own * scale_own**3 * jnp.mean(scaled_one * inputs_own, axis=-1, keepdims=True)
-    )
-    grad_input = grad_inputs.astype(BF16).reshape(1, rows, width)
-
     def placed(array, size):
         full = jnp.zeros((HEADS, size) + array.shape[1:], F32)
         return lax.dynamic_update_slice_in_dim(full, array[None], head, 0)
@@ -1101,26 +1322,62 @@
         ],
         axis=1,
     )
-    share = halved(halved(terms, "seq"), "batch")[0]
+    inputs_own = input_own.astype(F32)
+    if ring == 4:
+        padded = jnp.pad(terms, ((0, 0), (0, -terms.shape[1] % 1024)))
+        outs = finish(
+            lines,
+            term_pre.reshape(ring, lines, own, width),
+            term_output.reshape(lines, own, width),
+            after(grad_normed.astype(BF16), layer_output).reshape(ring, rows, width),
+            feed_sum.reshape(2, ring, own, hidden_part),
+            padded.reshape(ring, lines, -1, 128),
+            input_own,
+            gain_one[None],
+            grad_hidden,
+        )
+        query_share, key_share, value_share, swish_share, output_share, gate_share, up_share = outs[:7]
+        grad_input, share = outs[7], outs[8].reshape(-1)[: terms.shape[1]]
+    else:
+        share = halved(halved(terms, "seq"), "batch")[0]
+        grad_normed = scattered(grad_normed.astype(BF16), ring)
+        scale_own = rms_scale(inputs_own)
+        scaled_one = grad_normed * gain_one
+        grad_input = (
+            grad_hidden
+            + scale_own * scaled_one
+            - inputs_own * scale_own**3 * jnp.mean(scaled_one * inputs_own, axis=-1, keepdims=True)
+        ).astype(BF16)
+        output_share = lax.psum_scatter(term_output, "batch", scatter_dimension=0, tiled=True)
+        pre_sum = lax.psum_scatter(line_major(term_pre), "batch", scatter_dimension=0, tiled=True)
+        pre_share = exchanged(pre_sum.reshape(ring, own, 4 * part), mine, ring)
+        pre_share = pre_share.reshape(ring, own, 4, part).transpose(2, 1, 0, 3)
+        pre_share = pre_share.reshape(4, own, width).astype(F32)
+        query_share, key_share, value_share, swish_share = pre_share
+        feed_share = feed_sum.reshape(2, ring, own, hidden_part).transpose(1, 0, 2, 3)
+        feed_share = exchanged(feed_share, mine, ring)
+        gate_share = feed_share[:, 0].transpose(1, 0, 2).reshape(own, -1).astype(F32)
+        up_share = feed_share[:, 1].transpose(1, 0, 2).reshape(own, -1).astype(F32)
+        output_share = output_share.astype(F32)
     mixer_share, head_share, feedgain_share, bias_share, expand_share, squeeze_share = jnp.split(
         share, cuts
     )
     return (
         layer_output,
-        grad_input,
+        grad_input.reshape(1, rows, width),
         mixer_share,
-        pre_share[0],
-        pre_share[1],
-        pre_share[2],
+        query_share,
+        key_share,
+        value_share,
         squeeze_share.reshape(own, RANK),
         expand_share.reshape(-1, RANK).T,
         bias_share,
         swish_share,
         head_share,
-        output_share.astype(F32),
+        output_share,
         feedgain_share,
-        gate_share.astype(F32),
-        up_share.astype(F32),
+        gate_share,
+        up_share,
         down_share.astype(F32),
     )
 

time: 815 us -> 728 us (0.89)
  waiting for transfers between devices: 199 us -> 44.3 us
  Pallas kernels: 291 us -> 379 us
  starting transfers between devices: 24.7 us -> 9.27 us
    pallas_call x1 -> x2, Pallas kernels: 109 us -> 193 us  [the longest x1 112 us: finish(): pl.pallas_call(functools.partial(finish_kernel, lines), out_shape=(square...]
    ppermute x17 -> x8, waiting for transfers between devices: 71.3 us -> 16 us  [swapped(): return lax.ppermute(block, 'seq', [(i, i ^ by) for i in range(ring)])]
    reduce_scatter x3 -> x0, waiting for transfers between devices: 41.4 us -> none  [the longest x1 30.1 us: local(): lax.psum_scatter(after(term_swish, feed_sum), 'batch', scatter_dimension=...]
    all_gather x2, waiting for transfers between devices: 29.2 us -> 5.75 us  [over_batch(): lax.all_gather(blocks.reshape(-1, columns), 'batch', axis=0, tiled=False)]
    all_gather x2, waiting for transfers between devices: 28.7 us -> 11.8 us  [the longest x1 11.8 us: local(): lax.all_gather(after(down_weight, feed_columns), 'batch', axis=0, tiled=T...]
    reduce_scatter x1, waiting for transfers between devices: 25.4 us -> 9.27 us  [local(): lax.psum_scatter(term_down, 'batch', scatter_dimension=0, tiled=True)]
    unnamed x195 -> x202, local copies, waits for them, and re-layouts: 41.9 us -> 54.3 us
    ppermute x17 -> x8, starting transfers between devices: 19.8 us -> 9.03 us  [swapped(): return lax.ppermute(block, 'seq', [(i, i ^ by) for i in range(ring)])]
  transfers between devices with their start and end apart: 31 -> 14, of which waited for: 19 -> 7; matrix products, arithmetic and copies ran while one was open for 28% -> 30% of each run, Pallas kernels for 22% -> 26%
where the time goes in v5:
time: 728 us; the launch traced here: 722 us
  Pallas kernels  379 us (52%)
  matrix products  152 us (21%)
  local copies, waits for them, and re-layouts  102 us (14%)
  waiting for transfers between devices  44.3 us (6%)
  other arithmetic  20.5 us (3%)
  between operations  15.3 us (2%)
  starting transfers between devices  9.27 us (1%)
    pallas_call x2, Pallas kernels, fold(): pl.pallas_call(functools.partial(fold_kernel, finish, len(given)), out_sh...  155 us
    pallas_call x1, Pallas kernels, finish(): pl.pallas_call(functools.partial(finish_kernel, lines), out_shape=(square...  112 us
    pallas_call x1, Pallas kernels, start(): pl.pallas_call(functools.partial(start_kernel, ring, lines), out_shape=(j...  80.9 us
    dot_general x8, matrix products, dot_nn(): lax.dot_general(left, right, (((1,), (0,)), ((), ())), preferred_element_...  55.5 us
    unnamed x202, local copies, waits for them, and re-layouts  54.3 us
    dot_general x8, matrix products, dot_nt(): lax.dot_general(left, right, (((1,), (1,)), ((), ())), preferred_element_...  51.5 us
    dot_general x7, matrix products, dot_tn(): lax.dot_general(left, right, (((0,), (0,)), ((), ())), preferred_element_...  44.8 us
    pallas_call x1, Pallas kernels, mixer_backward(): pl.pallas_call(kernel, out_shape=(jax.ShapeDtypeStruct((length, size), BF...  20.4 us
  transfers between devices with their start and end apart: 14, of which 7 were waited for; matrix products, arithmetic and copies ran while one was open for 30% of the time, Pallas kernels for 26%

profile of v5, /device:TPU:0, one launch (start us, length us, event | category | flops | bytes accessed | tf_op | source)
XLA Modules:
  0.0 721.8 jit_solution(16808626013152751731)
XLA Ops:
  9.6 2.8 concatenate.41
  20.5 80.9 %start.1 = (bf16[4,256,2048]{2,1,0:T(8,128)(2,1)S(1)}, bf16[4,8,64,1536]{3,2,1,0:T(8,128)(2,1)S(1)}, bf16[4,64,512]{2,1,0:T(8,128)(2,1)}, bf16[64,2048]{1,0:T(8,...) custom-call(bf16[256,2048]{1,0:T(8,128)(2,1)S(1)} %bitcast.122, ...), custom_call_target="tpu_custom_call" | custom-call | tf_op jit(solution)/shard_map/start/pallas_call | solution.py:579
  101.5 2.0 copy-done
  103.5 2.6 copy-done.43
  107.6 1.5 collective-permute-start
  109.8 3.1 fusion
  114.8 3.4 fusion.2
  118.2 11.5 %convolution_convert_fusion.4 = bf16[1024,1536]{1,0:T(8,128)(2,1)} fusion(bf16[1024,2048]{1,0:T(8,128)(2,1)S(1)} %bitcast.143, bf16[2048,1536]{1,0:T(8,128)(2,1)} %bitcast.132), kind=kOutput, calls=%fused_computation.27 | convolution fusion | flops 6444023808 | bytes 13631488 | tf_op jit(solution)/shard_map/dot_general | solution.py:25
  134.1 3.4 fusion.34
  138.5 1.5 collective-permute-start.2
  143.1 2.5 constant_dynamic-update-slice_fusion.3
  145.6 2.3 constant_dynamic-update-slice_fusion.2
  147.9 4.6 collective-permute-done.2
  153.3 2.8 collective-permute-done.3
  163.1 11.1 %mixer_forward.1 = (f32[1024,512]{1,0:T(8,128)S(1)}, f32[64,1024]{1,0:T(8,128)S(1)}, f32[64,1024]{1,0:T(8,128)S(1)}, f32[8,64,512]{2,1,0:T(8,128)S(1)}, f32[8,64,512]{2,1,0:T(8,128)S(1)}) custom-call(s32[1]{0:T(128)} %bitcast.mine, bf16[1024,512]{1,0:T(8,128)(2,1)S(1)} %copy-done.11, bf16[1024,512]{1,0:T(8,128)(2,1)S(1)} %copy-done.9, ...), custom_call_target="tpu_custom_call" | custom-call | flops 1048576000 | bytes 6291456 | tf_op jit(solution)/shard_map/mixer_forward/pallas_call | solution.py:311
  178.3 1.9 copy.79
  180.2 1.4 copy-done.57
  181.6 4.2 multiply_convert_fusion.5
  185.8 4.3 convolution_convert_fusion.6
  190.2 74.9 %fold_forward.1 = (bf16[4,256,2048]{2,1,0:T(8,128)(2,1)S(1)}, f32[256,2048]{1,0:T(8,128)S(1)}) custom-call(bf16[4,256,2048]{2,1,0:T(8,128)(2,1)S(1)} %bitcast.124, bf16[256,2048]{1,0:T(8,128)(2,1)S(1)} %bitcast.123, f32[1,2048]{1,0:T(1,128)S(1)} %reshape.391.refs_2_.refs_3_), custom_call_target="tpu_custom_call" | custom-call | tf_op jit(solution)/shard_map/fold_forward/pallas_call | solution.py:967
  265.1 1.3 copy-done.5
  266.4 2.0 copy-done.45
  268.4 5.7 all-gather.9.cloned.1.call-done
  274.1 10.1 %fusion.32 = (bf16[1,4,8,64,1408]{4,3,1,0,2:T(8,128)(2,1)}, bf16[1,4,8,64,1408]{4,3,1,0,2:T(8,128)(2,1)}) fusion(bf16[2,4,8,64,1408]{4,3,1,0,2:T(8,128)(2,1)} %bitcast.147), kind=kLoop, calls=%fused_computation.101 | loop fusion | bytes 23068672 | tf_op jit(solution)/shard_map/unstack | solution.py:1166
  284.2 3.3 copy.82
  288.7 3.3 copy.83
  293.8 8.4 %fusion.36 = f32[1024,1408]{1,0:T(8,128)} fusion(bf16[1024,2048]{1,0:T(8,128)(2,1)S(1)} %bitcast.138, bf16[2048,1408]{1,0:T(8,128)(2,1)S(1)} %bitcast.149), kind=kOutput, calls=%fused_computation.105 | convolution fusion | flops 5905580032 | bytes 15728640 | tf_op jit(solution)/shard_map/dot_general | solution.py:25
  302.2 10.7 %multiply_convert_fusion.3 = (bf16[1024,1408]{1,0:T(8,128)(2,1)S(1)}, f32[1024,1408]{1,0:T(8,128)}) fusion(f32[1024,1408]{1,0:T(8,128)} %fusion.36, bf16[1024,2048]{1,0:T(8,128)(2,1)S(1)} %bitcast.139, bf16[2048,1408]{1,0:T(8,128)(2,1)S(1)} %bitcast.152), kind=kOutput, calls=%fused_computation.17 | convolution fusion | flops 5914230784 | bytes 24379392 | tf_op jit(solution)/shard_map/dot_general | solution.py:25
  312.9 1.5 copy-done.87
  314.4 8.1 %convolution_convert_fusion.3 = bf16[1408,2048]{1,0:T(8,128)(2,1)} fusion(bf16[1024,1408]{1,0:T(8,128)(2,1)S(1)} %get-tuple-element.182, bf16[1024,2048]{1,0:T(8,128)(2,1)S(1)} %copy-done.68), kind=kOutput, calls=%fused_computation.14 | convolution fusion | flops 5908463616 | bytes 12845056 | tf_op jit(solution)/shard_map/dot_general | solution.py:33
  322.6 11.8 %all-gather.11.cloned.1.call-done = bf16[1408,2048]{1,0:T(8,128)(2,1)} async-done(((bf16[176,2048]{1,0:T(8,128)(2,1)}), bf16[1408,2048]{1,0:T(8,128)(2,1)}) %all-gather.11.cloned.1.call-update) | async-done | bytes 5767184 | tf_op jit(solution)/shard_map/all_gather | solution.py:1167
  334.4 14.6 %multiply_convert_fusion.1 = (bf16[1024,1408]{1,0:T(8,128)(2,1)S(1)}, bf16[1024,1408]{1,0:T(8,128)(2,1)S(1)}) fusion(f32[1024,1408]{1,0:T(8,128)} %fusion.36, f32[1024,1408]{1,0:T(8,128)} %get-tuple-element.183, bf16[1024,2048]{1,0:T(8,128)(2,1)} %constant_dynamic-update-slice_fusion, bf16[1408,2048]{1,0:T(8,128)(2,1)} %all-gather.11.cloned.1.call-done), kind=kOutput, calls=%fused_computation.15 | convolution fusion | flops 5924323328 | bytes 27262976 | tf_op jit(solution)/shard_map/dot_general | solution.py:29
  349.0 8.8 %fusion.37 = f32[1024,2048]{1,0:T(8,128)S(1)} fusion(bf16[1024,1408]{1,0:T(8,128)(2,1)S(1)} %get-tuple-element.145, bf16[2048,1408]{1,0:T(8,128)(2,1)} %bitcast.150), kind=kOutput, calls=%fused_computation.106 | convolution fusion | flops 5905580032 | bytes 17039360 | tf_op jit(solution)/shard_map/dot_general | solution.py:29
  357.9 11.2 %add_convert_fusion = bf16[1024,2048]{1,0:T(8,128)(2,1)} fusion(f32[1024,2048]{1,0:T(8,128)S(1)} %fusion.37, bf16[1024,1408]{1,0:T(8,128)(2,1)S(1)} %get-tuple-element.144, bf16[2048,1408]{1,0:T(8,128)(2,1)} %bitcast.151), kind=kOutput, calls=%fused_computation.8 | convolution fusion | flops 5909774336 | bytes 21233664 | tf_op jit(solution)/shard_map/dot_general | solution.py:29
  369.1 7.1 convolution_convert_fusion.1
  376.2 7.3 %convolution_convert_fusion.2 = bf16[2048,1408]{1,0:T(8,128)(2,1)S(1)} fusion(bf16[1024,2048]{1,0:T(8,128)(2,1)S(1)} %bitcast.141, bf16[1024,1408]{1,0:T(8,128)(2,1)S(1)} %get-tuple-element.145), kind=kOutput, calls=%fused_computation.13 | convolution fusion | flops 5908463616 | bytes 12845056 | tf_op jit(solution)/shard_map/dot_general | solution.py:33
  383.5 1.9 maximum_bitcast_fusion
  385.4 5.5 copy.84
  390.8 9.3 %reduce-scatter.3.cloned.1.call-done = bf16[176,2048]{1,0:T(8,128)(2,1)} async-done(((bf16[1408,2048]{1,0:T(8,128)(2,1)}), bf16[176,2048]{1,0:T(8,128)(2,1)}) %reduce-scatter.3.cloned.1.call-update) | async-done | bytes 720912 | tf_op jit(solution)/shard_map/reduce_scatter | solution.py:1238
  401.5 9.7 %convolution_convert_fusion.5 = bf16[1024,2048]{1,0:T(8,128)(2,1)S(1)} fusion(bf16[1024,1408]{1,0:T(8,128)(2,1)} %copy-done.87, bf16[1408,2048]{1,0:T(8,128)(2,1)} %all-gather.11.cloned.1.call-done), kind=kOutput, calls=%fused_computation.28 | convolution fusion | flops 5907677184 | bytes 12845056 | tf_op jit(solution)/shard_map/dot_general | solution.py:25
  411.3 1.3 fusion.33
  412.6 1.5 collective-permute-start.4
  414.1 1.5 collective-permute-start.6
  415.6 79.8 %fold_backward.1 = (bf16[4,256,2048]{2,1,0:T(8,128)(2,1)S(1)}, f32[256,2048]{1,0:T(8,128)S(1)}, f32[1,2048]{1,0:T(1,128)S(1)}) custom-call(bf16[4,256,2048]{2,1,0:T(8,128)(2,1)S(1)} %bitcast.125, bf16[256,2048]{1,0:T(8,128)(2,1)S(1)} %bitcast.129, f32[256,2048]{1,0:T(8,128)S(1)} %copy-done.6, f32[1,2048]{1,0:T(1,128)S(1)} %reshape.391.refs_2_.refs_3_), custom_call_target="tpu_custom_call" | custom-call | tf_op jit(solution)/shard_map/fold_backward/pallas_call | solution.py:967
  495.4 3.1 multiply_reduce_fusion.1
  498.7 1.6 subtract_convert_fusion
  501.6 20.4 %mixer_backward.1 = (bf16[1024,512]{1,0:T(8,128)(2,1)S(1)}, bf16[1024,512]{1,0:T(8,128)(2,1)S(1)}, bf16[1024,512]{1,0:T(8,128)(2,1)S(1)}, f32[64,1024]{1,0:T(8,128)S(1)}) custom-call(s32[1]{0:T(128)} %bitcast.mine, bf16[1024,512]{1,0:T(8,128)(2,1)S(1)} %copy-done.12, bf16[1024,512]{1,0:T(8,128)(2,1)S(1)} %copy-done.10, ...), custom_call_target="tpu_custom_call" | custom-call | flops 2097152000 | bytes 10485760 | tf_op jit(solution)/shard_map/mixer_backward/pallas_call | solution.py:346
  523.1 2.4 fusion.38
  525.6 8.9 %fusion.11 = f32[1024,2048]{1,0:T(8,128)} fusion(bf16[2048,1536]{1,0:T(8,128)(2,1)S(1)} %bitcast.135, bf16[1024,512]{1,0:T(8,128)(2,1)S(1)} %get-tuple-element.77, bf16[1024,512]{1,0:T(8,128)(2,1)S(1)} %get-tuple-element.76, bf16[1024,512]{1,0:T(8,128)(2,1)S(1)} %get-tuple-element.75), kind=kOutput, calls=%fused_computation.30 | convolution fusion | flops 6451888128 | bytes 17825792 | tf_op jit(solution)/shard_map/dot_general | solution.py:29
  534.5 13.2 %convolution_convert_fusion = bf16[2048,2048]{1,0:T(8,128)(2,1)} fusion(bf16[1024,512]{1,0:T(8,128)(2,1)} %copy-done.63, bf16[1024,512]{1,0:T(8,128)(2,1)S(1)} %get-tuple-element.77, bf16[1024,512]{1,0:T(8,128)(2,1)S(1)} %get-tuple-element.76, bf16[1024,512]{1,0:T(8,128)(2,1)S(1)} %get-tuple-element.75, bf16[1024,2048]{1,0:T(8,128)(2,1)S(1)} %bitcast.119, ...), kind=kOutput, calls=%fused_computation.11 | convolution fusion | flops 8619294720 | bytes 16789504 | tf_op jit(solution)/shard_map/dot_general | solution.py:33
  547.8 6.5 multiply_reduce_fusion
  559.2 2.1 add_convert_fusion.3
  561.8 1.5 collective-permute-start.5
  563.4 1.8 fusion.18
  566.7 6.4 convolution_convert_fusion.7
  573.1 8.2 %collective-permute-done.7 = bf16[256,2048]{1,0:T(8,128)(2,1)} collective-permute-done((bf16[256,2048]{1,0:T(8,128)(2,1)S(1)}, bf16[256,2048]{1,0:T(8,128)(2,1)}, u32[]{:S(2)}, u32[]{:S(2)}) %collective-permute-start.7) | collective-permute-done | bytes 1048608 | tf_op jit(solution)/shard_map/ppermute | solution.py:988
  581.8 3.5 fusion.20
  585.3 1.3 convert_element_type.290
  586.6 111.8 %finish.1 = (f32[64,2048]{1,0:T(8,128)}, f32[64,2048]{1,0:T(8,128)}, f32[64,2048]{1,0:T(8,128)}, f32[64,2048]{1,0:T(8,128)}, f32[64,2048]{1,0:T(8,128)}, /*index...) custom-call(bf16[4,8,64,2048]{3,2,1,0:T(8,128)(2,1)} %bitcast.148, ...), custom_call_target="tpu_custom_call" | custom-call | tf_op jit(solution)/shard_map/finish/pallas_call | solution.py:933
  698.4 1.4 fusion.35
  701.3 1.3 split.57
  704.0 2.3 copy.124
  706.3 2.0 copy.125
  708.3 1.9 copy.126
  (277 shorter events, 56.8 us)
Async XLA Ops:
  7.2 171.1 %all-gather.5.cloned.1.call-start = ((), (), s32[]{:S(2)}) async-start(), calls=%async_computation.2 | async-start | bytes 2359296 | tf_op jit(solution)/shard_map/all_gather | solution.py:1160
  20.5 87.1 %copy-start.13 = (bf16[1,256,2048]{2,1,0:T(8,128)(2,1)S(1)}, bf16[1,256,2048]{2,1,0:T(8,128)(2,1)}, u32[]{:S(2)}) copy-start(bf16[1,256,2048]{2,1,0:T(8,128)(2,1)} %param.40) | copy-start | bytes 3145732
  106.1 79.7 %all-gather.7.cloned.1.call-start = ((), (), s32[]{:S(2)}) async-start(), calls=%async_computation.3 | async-start | bytes 2359296 | tf_op jit(solution)/shard_map/all_gather | solution.py:1165
  106.8 167.3 %all-gather.9.cloned.1.call-start = ((), (), s32[]{:S(2)}) async-start(), calls=%async_computation.4 | async-start | bytes 12976128 | tf_op jit(solution)/shard_map/all_gather | solution.py:1160
  107.6 226.8 %all-gather.11.cloned.1.call-start = ((), (), s32[]{:S(2)}) async-start(), calls=%async_computation.5 | async-start | bytes 6488064 | tf_op jit(solution)/shard_map/all_gather | solution.py:1167
  107.6 33.7 %collective-permute-start = (bf16[256,2048]{1,0:T(8,128)(2,1)S(1)}, bf16[256,2048]{1,0:T(8,128)(2,1)}, u32[]{:S(2)}, u32[]{:S(2)}) collective-permute-start(bf16[256,2048]{1,0:T(8,128)(2,1)S(1)} %bitcast.126), channel_id=1, source_target_pairs={{0,8},{8,0},{16,24},{24,16},{1,9},{9,1},{17,25},{25,17},{2,10},{10... | collective-permute-start | bytes 3145736 | tf_op jit(solution)/shard_map/ppermute | solution.py:988
  109.1 28.3 %collective-permute-start.1 = (bf16[256,2048]{1,0:T(8,128)(2,1)S(1)}, bf16[256,2048]{1,0:T(8,128)(2,1)}, u32[]{:S(2)}, u32[]{:S(2)}) collective-permute-start(bf16[256,2048]{1,0:T(8,128)(2,1)S(1)} %bitcast.127), channel_id=1, source_target_pairs={{0,16},{8,24},{16,0},{24,8},{1,17},{9,25},{17,1},{25,9},{2,18},{10... | collective-permute-start | bytes 3145736 | tf_op jit(solution)/shard_map/ppermute | solution.py:988
  109.8 290.4 %reduce-scatter.3.cloned.1.call-start = ((), (), s32[]{:S(2)}) async-start(), calls=%async_computation.6 | async-start | bytes 6488064 | tf_op jit(solution)/shard_map/reduce_scatter | solution.py:1238
  113.8 4.4 copy-start.82
  114.8 14.9 %copy-start.53 = (bf16[2048,16]{1,0:T(8,128)(2,1)}, bf16[2048,16]{1,0:T(8,128)(2,1)S(1)}, u32[]{:S(2)}) copy-start(bf16[2048,16]{1,0:T(8,128)(2,1)S(1)} %reshape.362) | copy-start | bytes 196612
  118.2 11.5 %copy-start.48 = (bf16[4,256,2048]{2,1,0:T(8,128)(2,1)}, bf16[4,256,2048]{2,1,0:T(8,128)(2,1)S(1)}, u32[]{:S(2)}) copy-start(bf16[4,256,2048]{2,1,0:T(8,128)(2,1)S(1)} %fusion.2) | copy-start | bytes 12582916
  130.9 6.6 copy-start.70
  131.6 5.8 copy-start.76
  138.5 18.4 %copy-start.24 = (f32[128,640]{1,0:T(8,128)S(1)}, f32[128,640]{1,0:T(8,128)}, u32[]{:S(2)}) copy-start(f32[128,640]{1,0:T(8,128)} %constant.82.clone.sums) | copy-start | bytes 983044
  138.5 13.9 %collective-permute-start.2 = (bf16[128,2048]{1,0:T(8,128)(2,1)S(1)}, bf16[128,2048]{1,0:T(8,128)(2,1)S(1)}, u32[]{:S(2)}, u32[]{:S(2)}) collective-permute-start(bf16[128,2048]{1,0:T(8,128)(2,1)S(1)} %slice.94), channel_id=1, source_target_pairs={{0,8},{8,0},{16,24},{24,16},{1,9},{9,1},{17,25},{25,17},{2,10},{10... | collective-permute-start | bytes 1572872 | tf_op jit(solution)/shard_map/ppermute | solution.py:988
  141.3 15.6 %copy-start.16 = (f32[1,1024]{0,1:T(8,128)S(1)}, f32[1,1024]{0,1:T(8,128)}, u32[]{:S(2)}) copy-start(f32[1,1024]{0,1:T(8,128)} %copy.100) | copy-start | bytes 12292
  142.5 13.6 %collective-permute-start.3 = (bf16[128,2048]{1,0:T(8,128)(2,1)S(1)}, bf16[128,2048]{1,0:T(8,128)(2,1)S(1)}, u32[]{:S(2)}, u32[]{:S(2)}) collective-permute-start(bf16[128,2048]{1,0:T(8,128)(2,1)S(1)} %slice.95), channel_id=1, source_target_pairs={{0,16},{8,24},{16,0},{24,8},{1,17},{9,25},{17,1},{25,9},{2,18},{10... | collective-permute-start | bytes 1572872 | tf_op jit(solution)/shard_map/ppermute | solution.py:988
  178.3 3.3 copy-start.49
  185.8 4.3 copy-start.4
  284.2 4.4 copy-start.50
  287.5 5.3 copy-start.51
  288.7 5.1 copy-start.46
  293.8 8.4 %copy-start.52 = (bf16[1,4,8,64,1408]{4,3,2,1,0:T(8,128)(2,1)S(1)}, bf16[1,4,8,64,1408]{4,3,2,1,0:T(8,128)(2,1)}, u32[]{:S(2)}) copy-start(bf16[1,4,8,64,1408]{4,3,2,1,0:T(8,128)(2,1)} %copy.83) | copy-start | bytes 17301508
  302.2 12.2 %copy-start.68 = (bf16[1024,2048]{1,0:T(8,128)(2,1)S(1)}, bf16[1024,2048]{1,0:T(8,128)(2,1)}, u32[]{:S(2)}) copy-start(bf16[1024,2048]{1,0:T(8,128)(2,1)} %constant_dynamic-update-slice_fusion) | copy-start | bytes 12582916
  322.6 264.0 %reduce-scatter.5.cloned.1.call-start = ((), (), s32[]{:S(2)}) async-start(), calls=%async_computation.7 | async-start | bytes 12976128 | tf_op jit(solution)/shard_map/reduce_scatter | solution.py:1241
  357.8 11.2 %copy-start.47 = (bf16[4,256,2048]{2,1,0:T(8,128)(2,1)S(1)}, bf16[4,256,2048]{2,1,0:T(8,128)(2,1)}, u32[]{:S(2)}) copy-start(bf16[4,256,2048]{2,1,0:T(8,128)(2,1)} %copy-done.45) | copy-start | bytes 12582916
  401.5 14.0 %copy-start.8 = (bf16[1024,2048]{1,0:T(8,128)(2,1)S(1)}, bf16[1024,2048]{1,0:T(8,128)(2,1)}, u32[]{:S(2)}) copy-start(bf16[1024,2048]{1,0:T(8,128)(2,1)} %add_convert_fusion) | copy-start | bytes 12582916
  411.2 4.3 copy-start.55
  411.2 4.3 copy-start.6
  411.2 4.3 copy-start.14
  412.6 82.8 %copy-start.56 = (f32[1024,512]{1,0:T(8,128)S(1)}, f32[1024,512]{1,0:T(8,128)}, u32[]{:S(2)}) copy-start(f32[1024,512]{1,0:T(8,128)} %get-tuple-element.181) | copy-start | bytes 6291460
  412.6 82.8 %copy-start.86 = (bf16[512,2048]{1,0:T(8,128)(2,1)S(1)}, bf16[512,2048]{1,0:T(8,128)(2,1)}, u32[]{:S(2)}) copy-start(bf16[512,2048]{1,0:T(8,128)(2,1)} %all-gather.7.cloned.1.call-done) | copy-start | bytes 6291460
  412.6 146.6 %collective-permute-start.4 = (bf16[128,2048]{1,0:T(8,128)(2,1)}, bf16[128,2048]{1,0:T(8,128)(2,1)}, u32[]{:S(2)}, u32[]{:S(2)}) collective-permute-start(bf16[128,2048]{1,0:T(8,128)(2,1)} %get-tuple-element.155), channel_id=1, source_target_pairs={{0,16},{8,24},{16,0},{24,8},{1,17},{9,25},{17,1},{25,9},{2,18},{10... | collective-permute-start | bytes 1572872 | tf_op jit(solution)/shard_map/ppermute | solution.py:988
  414.1 145.1 %collective-permute-start.6 = (bf16[128,2048]{1,0:T(8,128)(2,1)}, bf16[128,2048]{1,0:T(8,128)(2,1)}, u32[]{:S(2)}, u32[]{:S(2)}) collective-permute-start(bf16[128,2048]{1,0:T(8,128)(2,1)} %get-tuple-element.154), channel_id=1, source_target_pairs={{0,8},{8,0},{16,24},{24,16},{1,9},{9,1},{17,25},{25,17},{2,10},{10... | collective-permute-start | bytes 1572872 | tf_op jit(solution)/shard_map/ppermute | solution.py:988
  495.4 3.2 copy-start.15
  495.4 3.2 copy-start.44
  495.4 3.2 copy-start.84
  500.4 22.7 %copy-start.63 = (bf16[1024,512]{1,0:T(8,128)(2,1)}, bf16[1024,512]{1,0:T(8,128)(2,1)S(1)}, u32[]{:S(2)}) copy-start(bf16[1024,512]{1,0:T(8,128)(2,1)S(1)} %get-tuple-element.151) | copy-start | bytes 3145732
  501.6 20.4 %copy-start.69 = (f32[64,1024]{1,0:T(8,128)S(1)}, f32[64,1024]{1,0:T(8,128)}, u32[]{:S(2)}) copy-start(f32[64,1024]{1,0:T(8,128)} %get-tuple-element.179) | copy-start | bytes 786436
  501.6 21.5 %copy-start.58 = (bf16[1,4,8,64,512]{4,3,2,1,0:T(8,128)(2,1)S(1)}, bf16[1,4,8,64,512]{4,3,2,1,0:T(8,128)(2,1)}, u32[]{:S(2)}) copy-start(bf16[1,4,8,64,512]{4,3,2,1,0:T(8,128)(2,1)} %copy-done.57) | copy-start | bytes 6291460
  501.6 23.9 %slice-start = ((s8[6291456]{0:T(1024)(128)(4,1)}), s8[2097152]{0:T(1024)(128)(4,1)S(1)}, s32[]{:S(2)}) async-start(s8[6291456]{0:T(1024)(128)(4,1)} %bitcast.133), calls=%async_computation.8 | async-start | bytes 4194304
  523.1 24.7 %copy-start.74 = (bf16[1024,16]{0,1:T(8,128)(2,1)}, bf16[1024,16]{0,1:T(8,128)(2,1)S(1)}, u32[]{:S(2)}) copy-start(bf16[1024,16]{0,1:T(8,128)(2,1)S(1)} %convolution_convert_fusion.8) | copy-start | bytes 98308
  525.5 9.0 %copy-start.1 = (bf16[4,256,2048]{2,1,0:T(8,128)(2,1)S(1)}, bf16[4,256,2048]{2,1,0:T(8,128)(2,1)}, u32[]{:S(2)}) copy-start(bf16[4,256,2048]{2,1,0:T(8,128)(2,1)} %copy-done) | copy-start | bytes 12582916
  525.5 9.0 %copy-start.83 = (f32[2048]{0:T(1024)S(1)}, f32[2048]{0:T(1024)}, u32[]{:S(2)}) copy-start(f32[2048]{0:T(1024)} %copy-done.82) | copy-start | bytes 24580
  534.5 13.2 %copy-start.54 = (bf16[2048,16]{1,0:T(8,128)(2,1)S(1)}, bf16[2048,16]{1,0:T(8,128)(2,1)}, u32[]{:S(2)}) copy-start(bf16[2048,16]{1,0:T(8,128)(2,1)} %copy-done.53) | copy-start | bytes 196612
  547.7 10.6 %copy-start.71 = (bf16[1024,16]{0,1:T(8,128)(2,1)S(1)}, bf16[1024,16]{0,1:T(8,128)(2,1)}, u32[]{:S(2)}) copy-start(bf16[1024,16]{0,1:T(8,128)(2,1)} %copy-done.70) | copy-start | bytes 98308
  547.7 13.5 %copy-start.60 = (bf16[128,2048]{1,0:T(8,128)(2,1)S(1)}, bf16[128,2048]{1,0:T(8,128)(2,1)}, u32[]{:S(2)}) copy-start(bf16[128,2048]{1,0:T(8,128)(2,1)} %get-tuple-element.153) | copy-start | bytes 1572868
  554.3 7.4 %copy-start.59 = (bf16[128,2048]{1,0:T(8,128)(2,1)S(1)}, bf16[128,2048]{1,0:T(8,128)(2,1)}, u32[]{:S(2)}) copy-start(bf16[128,2048]{1,0:T(8,128)(2,1)} %get-tuple-element.152) | copy-start | bytes 1572868
  559.2 4.2 copy-start.2
  559.2 4.2 copy-start.75
  561.3 20.0 %collective-permute-start.7 = (bf16[256,2048]{1,0:T(8,128)(2,1)S(1)}, bf16[256,2048]{1,0:T(8,128)(2,1)}, u32[]{:S(2)}, u32[]{:S(2)}) collective-permute-start(bf16[256,2048]{1,0:T(8,128)(2,1)S(1)} %pad_maximum_fusion.1), channel_id=1, source_target_pairs={{0,16},{8,24},{16,0},{24,8},{1,17},{9,25},{17,1},{25,9},{2,18},{10... | collective-permute-start | bytes 3145736 | tf_op jit(solution)/shard_map/ppermute | solution.py:988
  561.8 4.0 copy-start.77
  561.8 4.0 copy-start.78
  561.8 4.0 copy-start.79
  561.8 4.0 copy-start.80
  561.8 4.0 copy-start.81
  561.8 19.9 %collective-permute-start.5 = (bf16[256,2048]{1,0:T(8,128)(2,1)S(1)}, bf16[256,2048]{1,0:T(8,128)(2,1)}, u32[]{:S(2)}, u32[]{:S(2)}) collective-permute-start(bf16[256,2048]{1,0:T(8,128)(2,1)S(1)} %pad_maximum_fusion), channel_id=1, source_target_pairs={{0,8},{8,0},{16,24},{24,16},{1,9},{9,1},{17,25},{25,17},{2,10},{10... | collective-permute-start | bytes 3145736 | tf_op jit(solution)/shard_map/ppermute | solution.py:988
  566.7 15.0 %copy-start.7 = (f32[256,2048]{1,0:T(8,128)S(1)}, f32[256,2048]{1,0:T(8,128)}, u32[]{:S(2)}) copy-start(f32[256,2048]{1,0:T(8,128)} %copy-done.5) | copy-start | bytes 6291460
  573.1 12.2 %copy-start.64 = (bf16[176,2048]{1,0:T(8,128)(2,1)S(1)}, bf16[176,2048]{1,0:T(8,128)(2,1)}, u32[]{:S(2)}) copy-start(bf16[176,2048]{1,0:T(8,128)(2,1)} %reduce-scatter.3.cloned.1.call-done) | copy-start | bytes 2162692
  698.3 11.8 %copy-start.67 = (f32[64,2048]{1,0:T(8,128)S(1)}, f32[64,2048]{1,0:T(8,128)}, u32[]{:S(2)}) copy-start(f32[64,2048]{1,0:T(8,128)} %get-tuple-element.207) | copy-start | bytes 1572868
  698.3 12.6 %copy-start.66 = (f32[64,2048]{1,0:T(8,128)S(1)}, f32[64,2048]{1,0:T(8,128)}, u32[]{:S(2)}) copy-start(f32[64,2048]{1,0:T(8,128)} %get-tuple-element.211) | copy-start | bytes 1572868
  698.4 13.4 %copy-start.65 = (f32[64,2048]{1,0:T(8,128)S(1)}, f32[64,2048]{1,0:T(8,128)}, u32[]{:S(2)}) copy-start(f32[64,2048]{1,0:T(8,128)} %get-tuple-element.213) | copy-start | bytes 1572868
  698.4 14.2 %copy-start.62 = (f32[64,5632]{1,0:T(8,128)S(1)}, f32[64,5632]{1,0:T(8,128)}, u32[]{:S(2)}) copy-start(f32[64,5632]{1,0:T(8,128)} %get-tuple-element.215) | copy-start | bytes 4325380
  706.3 7.4 %copy-start.61 = (f32[64,5632]{1,0:T(8,128)S(1)}, f32[64,5632]{1,0:T(8,128)}, u32[]{:S(2)}) copy-start(f32[64,5632]{1,0:T(8,128)} %get-tuple-element.216) | copy-start | bytes 4325380
  (40 other events, 62.1 us)
Sparse Core Ops, SparseCore 0:
  106.2 28.3 all-gather.4
  136.2 28.5 all-gather.6
  166.4 107.6 all-gather.8
  275.6 58.7 all-gather.10
  336.5 63.5 reduce-scatter.2
  402.3 117.6 reduce-scatter.4

commit v6 on v5

--- a/solution.py
+++ b/solution.py
@@ -60,28 +60,44 @@
     return dot_nt(high, right) + dot_nt(rest, right)
 
 
-def chunk_tables():
-    at = np.arange(CHUNK)
-    sums, covers = [], []
-    half = SUB
-    while half < CHUNK:
-        right = (at // half) % 2 == 1
-        edge = (at // (2 * half)) * 2 * half + half - 1
-        low = np.where(right, edge, at)
-        high = np.where(right, at, edge)
-        sums.append((at[:, None] > low[None, :]) & (at[:, None] <= high[None, :]))
-        same = (at[:, None] // (2 * half)) == (at[None, :] // (2 * half))
-        covers.append(same & ~right[:, None] & right[None, :])
-        half *= 2
-    sums.append(at[:, None] <= at[None, :])
-    sums.append(at[:, None] > at[None, :])
-    apart = at[None, :] - at[:, None]
-    apart = np.where(at[None, :] // SUB == at[:, None] // SUB, apart, -1)
-    return (
-        np.concatenate(sums, axis=1).astype(np.float32),
-        np.stack(covers).astype(np.float32),
-        np.maximum(apart, -1).astype(np.int32),
-    )
+LEVELS = (CHUNK // SUB).bit_length() - 1
+
+
+def fill_tables(sums, covers, apart):
+    source = lax.broadcasted_iota(jnp.int32, (CHUNK, CHUNK), 0)
+    target = lax.broadcasted_iota(jnp.int32, (CHUNK, CHUNK), 1)
+
+    def group(at, size):
+        return jnp.bitwise_and(at, CHUNK - size)
+
+    for level in range(LEVELS):
+        half = SUB << level
+        right = jnp.bitwise_and(target, half) != 0
+        edge = group(target, 2 * half) + (half - 1)
+        low, high = jnp.where(right, edge, target), jnp.where(right, target, edge)
+        sums[:, level * CHUNK : (level + 1) * CHUNK] = jnp.where(
+            (source > low) & (source <= high), 1.0, 0.0
+        )
+        same = group(source, 2 * half) == group(target, 2 * half)
+        covers[level] = jnp.where(same & (jnp.bitwise_and(source, half) == 0) & right, 1.0, 0.0)
+    sums[:, LEVELS * CHUNK : (LEVELS + 1) * CHUNK] = jnp.where(source <= target, 1.0, 0.0)
+    sums[:, (LEVELS + 1) * CHUNK :] = jnp.where(source > target, 1.0, 0.0)
+    apart[...] = jnp.where(group(source, SUB) == group(target, SUB), target - source, -1)
+
+
+TABLES = [
+    pltpu.VMEM((CHUNK, (LEVELS + 2) * CHUNK), F32),
+    pltpu.VMEM((LEVELS, CHUNK, CHUNK), F32),
+    pltpu.VMEM((CHUNK, CHUNK), jnp.int32),
+]
+
+
+def same_document(rows):
+    source = lax.broadcasted_iota(jnp.int32, (CHUNK, CHUNK), 0)
+    target = lax.broadcasted_iota(jnp.int32, (CHUNK, CHUNK), 1)
+    number = rows[0:1, :]
+    column = jnp.sum(jnp.where(source == target, number, 0.0), axis=1, keepdims=True)
+    return column == number
 
 
 def rolled(value, by):
@@ -97,41 +113,23 @@
 
 
 def mixer_forward_kernel(
-    levels,
-    factor,
-    mine,
-    query,
-    key,
-    value,
-    rate,
-    inflow,
-    rows,
-    segment_col,
-    sums,
-    covers,
-    apart,
-    output,
-    attention_out,
-    logits_out,
-    key_start,
-    value_start,
-    key_state,
-    value_state,
+    factor, mine, query, key, value, rate, rows, output, choice_out, start_out, state, sums, covers, apart
 ):
+    levels = LEVELS
+
     @pl.when(pl.program_id(0) == 0)
     def _():
-        key_state[...] = jnp.zeros_like(key_state)
-        value_state[...] = jnp.zeros_like(value_state)
-
-    key_in, value_in = key_state[...], value_state[...]
-    key_start[0] = key_in
-    value_start[0] = value_in
+        state[...] = jnp.zeros_like(state)
+        fill_tables(sums, covers, apart)
+
+    key_in, value_in = state[:SLOTS, :], state[SLOTS:, :]
+    start_out[0] = state[...]
     q, k, v = query[...], key[...], value[...]
-    a, g = rate[...], inflow[...]
+    a, g = rate[:SLOTS, :], rate[SLOTS:, :]
     decay = exponents(a, sums[...])
     before, after = piece(decay, levels), piece(decay, levels + 1)
     carried = before * rows[1:2, :]
-    visible = segment_col[...] == rows[0:1, :]
+    visible = same_document(rows)
     scores = jnp.where(visible, dot_nt(k, q) * factor, 0.0)
     logits = carried * (split_nt(key_in, q) * factor)
     for level in range(levels):
@@ -150,8 +148,8 @@
         )
     attention = jnp.exp(logits - jnp.max(logits, axis=0, keepdims=True))
     attention = attention / jnp.sum(attention, axis=0, keepdims=True)
-    attention_out[...] = attention
-    logits_out[...] = logits
+    choice_out[:SLOTS, :] = attention
+    choice_out[SLOTS:, :] = logits
     mixing = jnp.zeros((CHUNK, CHUNK), F32)
     for level in range(levels):
         part = piece(decay, level)
@@ -167,53 +165,32 @@
     )
     ends = after * g * rows[2:3, :]
     keep = carried[:, CHUNK - 1 : CHUNK]
-    key_state[...] = keep * key_in + split_nn(ends, k)
-    value_state[...] = keep * value_in + split_nn(ends, v)
+    state[:SLOTS, :] = keep * key_in + split_nn(ends, k)
+    state[SLOTS:, :] = keep * value_in + split_nn(ends, v)
 
 
 def mixer_backward_kernel(
-    levels,
-    factor,
-    mine,
-    query,
-    key,
-    value,
-    grad_output,
-    rate,
-    inflow,
-    rows,
-    segment_col,
-    sums,
-    covers,
-    apart,
-    later,
-    attention_in,
-    logits_in,
-    key_start,
-    value_start,
-    grad_query,
-    grad_key,
-    grad_value,
-    grad_rate,
-    key_grad,
-    value_grad,
-    flow,
+    factor, mine, query, key, value, grad_output, rate, rows, choice, start, grad_all, grad_rate,
+    state_grad, flow, sums, covers, apart,
 ):
+    levels = LEVELS
+
     @pl.when(pl.program_id(0) == 0)
     def _():
-        key_grad[...] = jnp.zeros_like(key_grad)
-        value_grad[...] = jnp.zeros_like(value_grad)
+        state_grad[...] = jnp.zeros_like(state_grad)
         flow[...] = jnp.zeros_like(flow)
-
-    key_in, value_in = key_start[0], value_start[0]
-    key_after, value_after = key_grad[...], value_grad[...]
+        fill_tables(sums, covers, apart)
+
+    key_in, value_in = start[0, :SLOTS, :], start[0, SLOTS:, :]
+    key_after, value_after = state_grad[:SLOTS, :], state_grad[SLOTS:, :]
     q, k, v, d = query[...], key[...], value[...], grad_output[...]
-    a, g = rate[...], inflow[...]
-    attention, logits = attention_in[...], logits_in[...]
+    size = q.shape[1]
+    a, g = rate[:SLOTS, :], rate[SLOTS:, :]
+    attention, logits = choice[:SLOTS, :], choice[SLOTS:, :]
     decay = exponents(a, sums[...])
     before, after = piece(decay, levels), piece(decay, levels + 1)
     carried = before * rows[1:2, :]
-    visible = segment_col[...] == rows[0:1, :]
+    visible = same_document(rows)
     scores = jnp.where(visible, dot_nt(k, q) * factor, 0.0)
     reads = jnp.where(visible, dot_nt(v, d), 0.0)
     gap = apart[...]
@@ -259,20 +236,21 @@
     log_carried = carried * grad_logits * factor
     att_carried = carried * attention
     ends = (ends * g).astype(BF16)
-    grad_query[...] = (
+    grad_all[:, :size] = (
         dot_tn(spread, k) + dot_tn(log_carried.astype(BF16), key_in.astype(BF16))
     ).astype(BF16)
-    grad_key[...] = (dot_nn(spread, q) + dot_tn(ends, key_after.astype(BF16))).astype(BF16)
-    grad_value[...] = (dot_nn(mixing, d) + dot_tn(ends, value_after.astype(BF16))).astype(BF16)
+    grad_all[:, size : 2 * size] = (dot_nn(spread, q) + dot_tn(ends, key_after.astype(BF16))).astype(BF16)
+    grad_all[:, 2 * size :] = (dot_nn(mixing, d) + dot_tn(ends, value_after.astype(BF16))).astype(BF16)
     change = grad_logits * logits + attention * grad_att - g * grad_inflow
-    same = jnp.where(visible, later[...], 0.0)
+    later = piece(sums, levels + 1) + jnp.where(gap == 0, 1.0, 0.0)
+    same = jnp.where(visible, later, 0.0)
     flows = exact_nn(change, same) + rows[2:3, :] * flow[:, 0:1]
     grad_rate[...] = rows[3:4, :] * flows - jnp.exp(a) * grad_inflow
     keep = carried[:, CHUNK - 1 : CHUNK]
     key_before = keep * key_after + split_nn(log_carried, q)
     value_before = keep * value_after + split_nn(att_carried, d)
-    key_grad[...] = key_before
-    value_grad[...] = value_before
+    state_grad[:SLOTS, :] = key_before
+    state_grad[SLOTS:, :] = value_before
     flow[...] = jnp.broadcast_to(
         jnp.sum(key_before * key_in + value_before * value_in, axis=1, keepdims=True), flow.shape
     )
@@ -289,88 +267,66 @@
         at = natural(step)
         return lax.bitwise_xor(at // per, mine[0]) * per + at % per
 
-    wide = pl.BlockSpec((CHUNK, size), lambda step, mine: (moved(step, mine), 0))
+    wide = [
+        pl.BlockSpec((CHUNK, size), lambda step, mine, at=at: (moved(step, mine), at))
+        for at in range(3)
+    ]
+    everything = pl.BlockSpec((CHUNK, 3 * size), lambda step, mine: (moved(step, mine), 0))
+    pair = pl.BlockSpec((2 * SLOTS, CHUNK), lambda step, mine: (0, moved(step, mine)))
     slim = pl.BlockSpec((SLOTS, CHUNK), lambda step, mine: (0, moved(step, mine)))
-    plain = pl.BlockSpec((SLOTS, CHUNK), lambda step, mine: (0, natural(step)))
     rows = pl.BlockSpec((8, CHUNK), lambda step, mine: (0, natural(step)))
-    column = pl.BlockSpec((CHUNK, 1), lambda step, mine: (natural(step), 0))
-    state = pl.BlockSpec((1, SLOTS, size), lambda step, mine: (natural(step), 0, 0))
-    return count, wide, slim, plain, rows, column, state
-
-
-def whole(array):
-    rank = array.ndim
-    return pl.BlockSpec(array.shape, lambda step, mine: (0,) * rank)
-
-
-def mixer_forward(mine, ring, query, key, value, rate, inflow, rows, column):
-    length, size = query.shape
-    sums, covers, apart = (jnp.asarray(table) for table in chunk_tables())
-    count, wide, slim, plain, row_spec, col_spec, state = mixer_specs(length, size, ring, False)
-    kernel = functools.partial(mixer_forward_kernel, covers.shape[0], size ** (-0.25))
+    state = pl.BlockSpec((1, 2 * SLOTS, size), lambda step, mine: (natural(step), 0, 0))
+    return count, wide, everything, pair, slim, rows, state
+
+
+def mixer_forward(mine, ring, joined, rates, rows):
+    length, size = joined.shape[0], joined.shape[1] // 3
+    count, wide, _, pair, _, row_spec, state = mixer_specs(length, size, ring, False)
     return pl.pallas_call(
-        kernel,
+        functools.partial(mixer_forward_kernel, size ** (-0.25)),
         out_shape=(
             jax.ShapeDtypeStruct((length, size), F32),
-            jax.ShapeDtypeStruct((SLOTS, length), F32),
-            jax.ShapeDtypeStruct((SLOTS, length), F32),
-            jax.ShapeDtypeStruct((count, SLOTS, size), F32),
-            jax.ShapeDtypeStruct((count, SLOTS, size), F32),
+            jax.ShapeDtypeStruct((2 * SLOTS, length), F32),
+            jax.ShapeDtypeStruct((count, 2 * SLOTS, size), F32),
         ),
         grid_spec=pltpu.PrefetchScalarGridSpec(
             num_scalar_prefetch=1,
             grid=(count,),
-            in_specs=[
-                wide, wide, wide, slim, slim, row_spec, col_spec,
-                whole(sums), whole(covers), whole(apart),
-            ],
-            out_specs=[wide, plain, plain, state, state],
-            scratch_shapes=[pltpu.VMEM((SLOTS, size), F32)] * 2,
+            in_specs=wide + [pair, row_spec],
+            out_specs=[wide[0], pair, state],
+            scratch_shapes=[pltpu.VMEM((2 * SLOTS, size), F32)] + TABLES,
         ),
         compiler_params=pltpu.CompilerParams(vmem_limit_bytes=32 << 20),
         cost_estimate=pl.CostEstimate(
             flops=length * size * 2000, bytes_accessed=length * size * 12, transcendentals=length * 4096
         ),
         name="mixer_forward",
-    )(mine, query, key, value, rate, inflow, rows, column, sums, covers, apart)
-
-
-def mixer_backward(
-    mine, ring, query, key, value, grad, rate, inflow, rows, column, attention, logits, starts
-):
-    length, size = query.shape
-    sums, covers, apart = (jnp.asarray(table) for table in chunk_tables())
-    later = jnp.asarray(np.tril(np.ones((CHUNK, CHUNK), np.float32)))
-    count, wide, slim, plain, row_spec, col_spec, state = mixer_specs(length, size, ring, True)
-    kernel = functools.partial(mixer_backward_kernel, covers.shape[0], size ** (-0.25))
+    )(mine, joined, joined, joined, rates, rows)
+
+
+def mixer_backward(mine, ring, joined, grad, rates, rows, choice, starts):
+    length, size = grad.shape
+    count, wide, everything, pair, slim, row_spec, state = mixer_specs(length, size, ring, True)
     return pl.pallas_call(
-        kernel,
+        functools.partial(mixer_backward_kernel, size ** (-0.25)),
         out_shape=(
-            jax.ShapeDtypeStruct((length, size), BF16),
-            jax.ShapeDtypeStruct((length, size), BF16),
-            jax.ShapeDtypeStruct((length, size), BF16),
+            jax.ShapeDtypeStruct((length, 3 * size), BF16),
             jax.ShapeDtypeStruct((SLOTS, length), F32),
         ),
         grid_spec=pltpu.PrefetchScalarGridSpec(
             num_scalar_prefetch=1,
             grid=(count,),
-            in_specs=[
-                wide, wide, wide, wide, slim, slim, row_spec, col_spec,
-                whole(sums), whole(covers), whole(apart), whole(later),
-                plain, plain, state, state,
-            ],
-            out_specs=[wide, wide, wide, slim],
-            scratch_shapes=[pltpu.VMEM((SLOTS, size), F32)] * 2 + [pltpu.VMEM((SLOTS, 128), F32)],
+            in_specs=wide + [wide[0], pair, row_spec, pair, state],
+            out_specs=[everything, slim],
+            scratch_shapes=[pltpu.VMEM((2 * SLOTS, size), F32), pltpu.VMEM((SLOTS, 128), F32)]
+            + TABLES,
         ),
         compiler_params=pltpu.CompilerParams(vmem_limit_bytes=32 << 20),
         cost_estimate=pl.CostEstimate(
             flops=length * size * 4000, bytes_accessed=length * size * 20, transcendentals=length * 4096
         ),
         name="mixer_backward",
-    )(
-        mine, query, key, value, grad, rate, inflow, rows, column,
-        sums, covers, apart, later, attention, logits, *starts,
-    )
+    )(mine, joined, joined, joined, grad, rates, rows, choice, starts)
 
 
 def peers(ring, mine):
@@ -464,7 +420,8 @@
 
 def start_kernel(
     ring, lines, inputs, w_query, w_key, w_value, w_swish, w_out, gate, up, small,
-    inputs_all, w_mixer, swish_columns, out_rows, feed_columns, small_all,
+    inputs_all, w_mixer, swish_columns, w_output, gate_columns, up_columns, small_all,
+    own_input, mixer_blocks, swish_blocks, own_out, gate_blocks, up_blocks,
     local_sem, send_sem, recv_sem,
 ):
     mine, batch = lax.axis_index("seq"), lax.axis_index("batch")
@@ -473,50 +430,45 @@
     part = swish_columns.shape[2]
     half = inputs.shape[0] // 2
     others = peers(ring, mine)
-    pieces = (w_query, w_key, w_value)
-
-    def column(ref, at):
-        if len(ref.shape) == 3:
-            return ref.at[at]
-        size = ref.shape[1] // ring
-        return ref.at[:, pl.ds(pl.multiple_of(at * size, 128), size)]
-
-    def slot(source, piece):
-        return w_mixer.at[source, batch, :, pl.ds(piece * part, part)]
-
-    near = [copies.near(column(ref, mine), slot(mine, at)) for at, ref in enumerate(pieces)]
-    near += [copies.near(small, small_all.at[mine, batch])]
-    column_waits, small_waits = [], []
-    for to in others:
-        column_waits.append(
-            [
-                copies.far(column(ref, to), slot(mine, at), slot(to, at), (to, batch))
-                for at, ref in enumerate(pieces)
-            ]
-        )
-        small_waits.append(
-            copies.far(small, small_all.at[mine, batch], small_all.at[to, batch], (to, batch))
-        )
+
+    def columns(ref, blocks, first, size):
+        return [
+            copies.near(
+                ref.at[at] if len(ref.shape) == 3 else ref.at[:, pl.ds(at * size, size)],
+                blocks.at[at, :, pl.ds(first, size)],
+            )
+            for at in range(ring)
+        ]
+
+    loads = []
+    for at, ref in enumerate((w_query, w_key, w_value)):
+        loads += columns(ref, mixer_blocks, at * part, part)
     direct = 2 if ring == 4 else ring - 1
-
-    def sent(block, blocks):
-        return copies.near(block, blocks.at[0]), [
-            copies.far(block, blocks.at[by + 1], blocks.at[by + 1], (others[by], batch))
-            for by in range(direct)
-        ]
-
-    def passed_on(blocks, waits):
-        for wait in waits:
-            wait()
-        if ring != 4:
-            return []
-        low, high = pl.ds(0, half), pl.ds(half, half)
-        return [
-            copies.far(blocks.at[have, rows], blocks.at[3, rows], blocks.at[3, rows], (to, batch))
-            for have, rows, to in ((2, low, others[0]), (1, high, others[1]))
-        ]
-
-    own_input, input_waits = sent(inputs, inputs_all)
+    input_waits = [
+        copies.far(inputs, inputs_all.at[by + 1], inputs_all.at[by + 1], (others[by], batch))
+        for by in range(direct)
+    ]
+    own_load = copies.near(inputs, own_input)
+    hidden = gate_columns.shape[2]
+    out_load = copies.near(w_out, own_out)
+    other_loads = columns(w_swish, swish_blocks, 0, part)
+    other_loads += columns(gate, gate_blocks, 0, hidden) + columns(up, up_blocks, 0, hidden)
+    for copy in loads:
+        copy.wait()
+    column_waits = [
+        copies.far(
+            mixer_blocks.at[to], w_mixer.at[mine, batch], w_mixer.at[to, batch], (to, batch)
+        )
+        for to in others
+    ]
+    near = [
+        copies.near(mixer_blocks.at[mine], w_mixer.at[mine, batch]),
+        copies.near(small, small_all.at[mine, batch]),
+    ]
+    small_waits = [
+        copies.far(small, small_all.at[mine, batch], small_all.at[to, batch], (to, batch))
+        for to in others
+    ]
     for copy in near:
         copy.wait()
 
@@ -527,43 +479,48 @@
 
     chains = []
     started(lambda at: w_mixer.at[mine, at])
-    for waits, source in zip(column_waits, others):
-        for wait in waits:
-            wait()
+    for wait, source in zip(column_waits, others):
+        wait()
         started(lambda at, source=source: w_mixer.at[source, at])
     for wait, source in zip(small_waits, others):
         wait()
         started(lambda at, source=source: small_all.at[source, at])
     started(lambda at: small_all.at[mine, at])
-    input_waits = passed_on(inputs_all, input_waits)
-    own_columns = [
-        copies.near(column(w_swish, mine), swish_columns.at[mine]),
-        copies.near(w_out, out_rows),
-    ]
-    own_columns += [
-        copies.near(column(ref, mine), feed_columns.at[at, mine]) for at, ref in enumerate((gate, up))
-    ]
+    out_load.wait()
+    near = copies.near(own_out, w_output.at[batch])
+    near.wait()
+    started(lambda at: w_output.at[at])
+    own_load.wait()
+    stores = [copies.near(own_input, inputs_all.at[0])]
+    for copy in other_loads:
+        copy.wait()
+    moved = (
+        (swish_blocks, swish_columns), (gate_blocks, gate_columns), (up_blocks, up_columns)
+    )
+    stores += [copies.near(blocks.at[mine], array.at[mine]) for blocks, array in moved]
+    for wait in input_waits:
+        wait()
+    if ring == 4:
+        low, high = pl.ds(0, half), pl.ds(half, half)
+        input_waits = [
+            copies.far(
+                inputs_all.at[have, rows], inputs_all.at[3, rows], inputs_all.at[3, rows], (to, batch)
+            )
+            for have, rows, to in ((2, low, others[0]), (1, high, others[1]))
+        ]
+    else:
+        input_waits = []
     other_waits = [
-        copies.far(column(w_swish, to), swish_columns.at[mine], swish_columns.at[to], (to, batch))
+        copies.far(blocks.at[to], array.at[mine], array.at[to], (to, batch))
+        for blocks, array in moved
         for to in others
     ]
-    other_waits += [
-        copies.far(
-            column(ref, to), feed_columns.at[at, mine], feed_columns.at[at, to], (to, batch)
-        )
-        for to in others
-        for at, ref in enumerate((gate, up))
-    ]
     for step in range(1, chips + 1):
-        for chain in chains:
-            if chips > 1 or step > 1:
-                next(chain)
-    if chips == 1:
         for chain in chains:
             next(chain)
     for wait in input_waits + other_waits:
         wait()
-    for copy in [own_input] + own_columns:
+    for copy in stores:
         copy.wait()
     copies.close()
 
@@ -573,23 +530,30 @@
     part, hidden = width // ring, gate.shape[1] // ring
     if hidden % 128:
         gate, up = (a.reshape(own, ring, hidden).transpose(1, 0, 2) for a in (gate, up))
-    inside, anywhere = (pl.BlockSpec(memory_space=space) for space in (pltpu.VMEM, pl.ANY))
-    chains = 2 * ring
-    away = (ring - 1) * 9 + 2 + chains * (4 * (lines // 2 - 1) + 1)
+    anywhere, outside = (pl.BlockSpec(memory_space=space) for space in (pl.ANY, pltpu.HBM))
+    away = (ring - 1) * 6 + 2 + (2 * ring + 1) * (4 * (lines // 2 - 1) + 1)
+    thin = (ring, own, hidden)
     return pl.pallas_call(
         functools.partial(start_kernel, ring, lines),
         out_shape=(
             jax.ShapeDtypeStruct((ring,) + inputs.shape, BF16),
             jax.ShapeDtypeStruct((ring, lines, own, 3 * part), BF16),
             jax.ShapeDtypeStruct((ring, own, part), BF16),
-            jax.ShapeDtypeStruct(w_out.shape, BF16),
-            jax.ShapeDtypeStruct((2, ring, own, hidden), BF16),
+            jax.ShapeDtypeStruct((lines,) + w_out.shape, BF16),
+            jax.ShapeDtypeStruct(thin, BF16),
+            jax.ShapeDtypeStruct(thin, BF16),
             jax.ShapeDtypeStruct((ring, lines) + small.shape, BF16),
         ),
-        in_specs=[inside] * 4 + [anywhere] * 4 + [inside],
-        out_specs=[anywhere] * 6,
+        in_specs=[anywhere] * 9,
+        out_specs=[outside] * 7,
         scratch_shapes=[
-            pltpu.SemaphoreType.DMA((12,)),
+            pltpu.VMEM(inputs.shape, BF16),
+            pltpu.VMEM((ring, own, 3 * part), BF16),
+            pltpu.VMEM((ring, own, part), BF16),
+            pltpu.VMEM(w_out.shape, BF16),
+            pltpu.VMEM(thin, BF16),
+            pltpu.VMEM(thin, BF16),
+            pltpu.SemaphoreType.DMA((6 * ring + 9,)),
             pltpu.SemaphoreType.DMA((away,)),
             pltpu.SemaphoreType.DMA((away,)),
         ],
@@ -681,15 +645,44 @@
     copies.close()
 
 
+def half_blocks(value, order):
+    lane = lax.broadcasted_iota(jnp.int32, (value.shape[0], 128), 1)
+    made = []
+    for pair in zip(order[::2], order[1::2]):
+        low, high = (
+            value[:, block * 128 : (block + 1) * 128]
+            if half == want
+            else pltpu.roll(value[:, block * 128 : (block + 1) * 128], 64, 1)
+            for want, (block, half) in enumerate(pair)
+        )
+        made.append(jnp.where(lane < 64, low, high))
+    return jnp.concatenate(made, axis=1)
+
+
+def by_line(value):
+    lines = value.shape[1] // 256
+    return half_blocks(
+        value, [divmod(ring * lines + line, 2) for line in range(lines) for ring in range(4)]
+    )
+
+
+def by_ring(value):
+    lines = value.shape[1] // 256
+    return half_blocks(
+        value, [divmod(line * 4 + ring, 2) for ring in range(4) for line in range(lines)]
+    )
+
+
 def finish_forward(total, full, at, given, made):
     inputs, gain = given
     hidden = inputs[full, :].astype(F32) + total
     made[0][full, :] = hidden
-    return (hidden * rms_scale(hidden) * gain[...]).astype(BF16)
+    return by_line(hidden * rms_scale(hidden) * gain[...]).astype(BF16)
 
 
 def finish_backward(total, full, at, given, made):
     cotangent, hidden_ref, gain = given
+    total = by_ring(total)
     hidden = hidden_ref[full, :]
     scale = rms_scale(hidden)
     plain = hidden * scale
@@ -706,7 +699,7 @@
 
 
 def finish_kernel(
-    lines, mixer_terms, out_terms, input_terms, feed_sum, small_terms, inputs, gain, grad_hidden,
+    lines, mixer_terms, out_terms, input_terms, gate_sum, up_sum, small_terms, inputs, gain, grad_hidden,
     grad_query, grad_key, grad_value, grad_swish, grad_out, grad_gate, grad_up, grad_input, small_sum,
     crossed, staged, arrived, summed, outgoing, mixer_blocks, feed_blocks, small_ring, small_mine, small_line,
     first, second, third, two_low, one_high, local_sem, send_sem, recv_sem,
@@ -737,8 +730,11 @@
         for at, to in enumerate(others)
     ]
     feed_waits = [
-        copies.far(feed_sum.at[:, to], feed_blocks.at[mine], feed_blocks.at[to], (to, batch))
+        copies.far(
+            array.at[to], feed_blocks.at[mine, at], feed_blocks.at[to, at], (to, batch)
+        )
         for to in others
+        for at, array in enumerate((gate_sum, up_sum))
     ]
 
     size = input_terms.shape[1] // PARTS
@@ -804,8 +800,9 @@
     def feed_part():
         for wait in feed_waits:
             wait()
-        feed_blocks[mine] = feed_sum[:, mine]
-        wide = feed_sum.shape[3]
+        feed_blocks[mine, 0] = gate_sum[mine]
+        feed_blocks[mine, 1] = up_sum[mine]
+        wide = gate_sum.shape[2]
         for source in range(4):
             at = pl.ds(source * wide, wide)
             grad_gate[:, at] = feed_blocks[source, 0].astype(F32)
@@ -920,14 +917,14 @@
     copies.close()
 
 
-def finish(lines, mixer_terms, out_terms, input_terms, feed_sum, small_terms, inputs, gain, grad_hidden):
+def finish(lines, mixer_terms, out_terms, input_terms, gate_sum, up_sum, small_terms, inputs, gain, grad_hidden):
     ring, _, own, width = mixer_terms.shape
-    rows, hidden = inputs.shape[0], feed_sum.shape[3]
+    rows, hidden = inputs.shape[0], gate_sum.shape[2]
     chips = lines // 2
     inside = pl.BlockSpec(memory_space=pltpu.VMEM)
     block = pltpu.VMEM((rows, width), BF16)
     small = small_terms.shape[2:]
-    away = (ring + 1) * (chips + 2 * (chips - 1)) + 3 * (ring - 1) + PARTS * 6 + lines - 1
+    away = (ring + 1) * (chips + 2 * (chips - 1)) + 4 * (ring - 1) + PARTS * 6 + lines - 1
     square = jax.ShapeDtypeStruct((own, width), F32)
     wide = jax.ShapeDtypeStruct((own, ring * hidden), F32)
     return pl.pallas_call(
@@ -935,7 +932,7 @@
         out_shape=(square,) * 5
         + (wide,) * 2
         + (jax.ShapeDtypeStruct((rows, width), BF16), jax.ShapeDtypeStruct(small, F32)),
-        in_specs=[inside] * 8,
+        in_specs=[inside] * 9,
         out_specs=[inside] * 9,
         scratch_shapes=[
             pltpu.VMEM((ring + 1, chips, own, width), BF16),
@@ -957,7 +954,7 @@
         ],
         compiler_params=pltpu.CompilerParams(has_side_effects=True, vmem_limit_bytes=58 << 20),
         name="finish",
-    )(mixer_terms, out_terms, input_terms, feed_sum, small_terms, inputs, gain, grad_hidden)
+    )(mixer_terms, out_terms, input_terms, gate_sum, up_sum, small_terms, inputs, gain, grad_hidden)
 
 
 def fold(finish, terms, given, made, name):
@@ -968,7 +965,7 @@
         functools.partial(fold_kernel, finish, len(given)),
         out_shape=(jax.ShapeDtypeStruct((ring, rows, width), BF16),) + made,
         in_specs=[inside] * (1 + len(given)),
-        out_specs=[pl.BlockSpec(memory_space=pl.ANY)] + [inside] * len(made),
+        out_specs=[pl.BlockSpec(memory_space=pltpu.HBM)] + [inside] * len(made),
         scratch_shapes=[block] * 6
         + [
             pltpu.SemaphoreType.DMA((PARTS,)),
@@ -1124,7 +1121,7 @@
     params = jnp.pad(params, (0, -params.shape[0] % 2048)).reshape(-1, 128)
     input_own = layer_input.reshape(rows, width)
     grad_own = cotangent.reshape(rows, width)
-    inputs, w_mixer, swish_columns, out_rows, feed_columns, small = start(
+    inputs, w_mixer, swish_columns, w_output, gate_columns, up_columns, small = start(
         ring,
         lines,
         input_own,
@@ -1155,16 +1152,22 @@
     )
     w_squeeze = w_squeeze.reshape(width, RANK).T
 
+    w_output = w_output.reshape(part, width)
+
     def over_batch(blocks):
-        kinds, columns = blocks.shape[0], blocks.shape[-1]
-        full = lax.all_gather(blocks.reshape(-1, columns), "batch", axis=0, tiled=False)
-        full = full.reshape(lines, kinds, ring, own, columns)
-        return full.transpose(1, 2, 0, 3, 4).reshape(kinds, width, columns)
-
-    w_swish = over_batch(swish_columns[None])[0]
-    w_output = lax.all_gather(out_rows, "batch", axis=0, tiled=True)
-    w_gate, w_up = over_batch(feed_columns)
-    w_down = lax.all_gather(after(down_weight, feed_columns), "batch", axis=0, tiled=True)
+        return lax.all_gather(blocks.reshape(ring * own, -1), "batch", axis=0, tiled=True)
+
+    def own_order(array):
+        return array.reshape(lines, ring, own, -1).transpose(1, 0, 2, 3).reshape(width, -1)
+
+    def line_major(term):
+        return term.reshape(ring, lines, own, -1).transpose(1, 0, 2, 3).reshape(width, -1)
+
+    w_swish = own_order(over_batch(swish_columns))
+    w_gate, w_up = over_batch(gate_columns), over_batch(up_columns)
+    if ring != 4:
+        w_gate, w_up = own_order(w_gate), own_order(w_up)
+    w_down = lax.all_gather(after(down_weight, gate_columns), "batch", axis=0, tiled=True)
 
     chunked = segment.reshape(-1, CHUNK)
     before = jnp.concatenate([jnp.full((1,), -1.0, F32), chunked[:-1, -1]])
@@ -1178,26 +1181,25 @@
         ]
         + [jnp.zeros_like(segment)] * 4
     )
-    segment_col = segment[:, None]
 
     inputs = inputs.astype(F32)
     scale_one = rms_scale(inputs)
     plain_one = inputs * scale_one
     normed = (plain_one * gain_one).astype(BF16)
     mixer_pre = dot_nn(normed, w_mixer)
-    query = whole_head(mixer_pre[:, :part].astype(BF16))
-    key = whole_head(mixer_pre[:, part : 2 * part].astype(BF16))
-    value = whole_head(mixer_pre[:, 2 * part : 3 * part].astype(BF16))
+    joined = mixer_pre.astype(BF16)
+    if copies > 1:
+        joined = jnp.concatenate(
+            [whole_head(joined[:, at * part : (at + 1) * part]) for at in range(3)], axis=1
+        )
     swish_pre = whole_head(dot_nn(normed, w_swish))
     reduced = dot_nt(normed, w_squeeze).astype(BF16)
     forget_logit = dot_nt(expand_head, reduced) + bias_head.astype(F32)[:, None]
     log_rate = jax.nn.log_sigmoid(forget_logit) / TAU_GATE
-    inflow = -jnp.expm1(log_rate)
+    rates = jnp.concatenate([log_rate, -jnp.expm1(log_rate)], axis=0)
     order = mine.reshape(1).astype(jnp.int32)
-    query, grad_out = lax.optimization_barrier((query, grad_out))
-    mixed, attention, logits, key_start, value_start = mixer_forward(
-        order, ring, query, key, value, log_rate, inflow, mask_rows, segment_col
-    )
+    mixed, choice, starts = mixer_forward(order, ring, joined, rates, mask_rows)
+    mixed, grad_out = lax.optimization_barrier((mixed, grad_out))
     head_factor = rms_scale(mixed)
     head_plain = mixed * head_factor
     head_normed = head_plain * gain_head
@@ -1236,15 +1238,18 @@
     result = hidden + scattered(result_terms, ring)
     layer_output = result.astype(BF16).reshape(1, rows, width)
     down_share = lax.psum_scatter(term_down, "batch", scatter_dimension=0, tiled=True)
-    term_feedpre = jnp.stack([term_gate, term_up]).reshape(2, ring, lines, own, hidden_part)
-    term_feedpre = term_feedpre.transpose(2, 0, 1, 3, 4).reshape(-1, hidden_part)
-    feed_sum = lax.psum_scatter(
-        after(term_feedpre, down_share), "batch", scatter_dimension=0, tiled=True
+    if ring != 4:
+        term_gate, term_up = line_major(term_gate), line_major(term_up)
+    gate_sum = lax.psum_scatter(
+        after(term_gate, down_share), "batch", scatter_dimension=0, tiled=True
+    )
+    up_sum = lax.psum_scatter(
+        after(term_up, down_share), "batch", scatter_dimension=0, tiled=True
     )
     if ring == 4:
         grad_branch, grad_hidden, term_feed = fold(
             finish_backward,
-            after(back_feedin, term_feedpre).reshape(ring, rows, width),
+            after(back_feedin, term_gate, term_up).reshape(ring, rows, width),
             (grad_own, hidden, gain_two[None]),
             (
                 jax.ShapeDtypeStruct((rows, width), F32),
@@ -1268,9 +1273,6 @@
     grad_gated = whole_head(dot_nt(grad_branch, w_output))
     term_output = dot_tn(gated, grad_branch).astype(BF16)
 
-    def line_major(term):
-        return term.reshape(ring, lines, own, -1).transpose(1, 0, 2, 3).reshape(width, -1)
-
     slope = swish_sig * (1.0 + swish_pre * (1.0 - swish_sig))
     grad_swishpre = own_part((grad_gated * head_normed * slope).astype(BF16))
     grad_normed_head = grad_gated * swish_act
@@ -1279,28 +1281,17 @@
     grad_mixed = head_factor * scaled_head - mixed * head_factor**3 * jnp.mean(
         scaled_head * mixed, axis=-1, keepdims=True
     )
-    grad_query, grad_key, grad_value, grad_rate = mixer_backward(
-        order,
-        ring,
-        query,
-        key,
-        value,
-        grad_mixed.astype(BF16),
-        log_rate,
-        inflow,
-        mask_rows,
-        segment_col,
-        attention,
-        logits,
-        (key_start, value_start),
+    grad_pre, grad_rate = mixer_backward(
+        order, ring, joined, grad_mixed.astype(BF16), rates, mask_rows, choice, starts
     )
     grad_logit = (grad_rate * jax.nn.sigmoid(-forget_logit) / TAU_GATE).astype(BF16)
     term_bias = jnp.sum(grad_logit.astype(F32), axis=1) / copies
     term_expand = dot_nn(grad_logit, reduced) / copies
     grad_reduced = (dot_tn(grad_logit, expand_head) / copies).astype(BF16)
-    grad_pre = jnp.concatenate(
-        [own_part(grad_query), own_part(grad_key), own_part(grad_value)], axis=1
-    )
+    if copies > 1:
+        grad_pre = jnp.concatenate(
+            [own_part(grad_pre[:, at * head_size : (at + 1) * head_size]) for at in range(3)], axis=1
+        )
     grad_normed = (
         dot_nt(grad_pre, w_mixer) + dot_nt(grad_swishpre, w_swish) + dot_nn(grad_reduced, w_squeeze)
     )
@@ -1330,7 +1321,8 @@
             term_pre.reshape(ring, lines, own, width),
             term_output.reshape(lines, own, width),
             after(grad_normed.astype(BF16), layer_output).reshape(ring, rows, width),
-            feed_sum.reshape(2, ring, own, hidden_part),
+            gate_sum.reshape(ring, own, hidden_part),
+            up_sum.reshape(ring, own, hidden_part),
             padded.reshape(ring, lines, -1, 128),
             input_own,
             gain_one[None],
@@ -1354,10 +1346,13 @@
         pre_share = pre_share.reshape(ring, own, 4, part).transpose(2, 1, 0, 3)
         pre_share = pre_share.reshape(4, own, width).astype(F32)
         query_share, key_share, value_share, swish_share = pre_share
-        feed_share = feed_sum.reshape(2, ring, own, hidden_part).transpose(1, 0, 2, 3)
-        feed_share = exchanged(feed_share, mine, ring)
-        gate_share = feed_share[:, 0].transpose(1, 0, 2).reshape(own, -1).astype(F32)
-        up_share = feed_share[:, 1].transpose(1, 0, 2).reshape(own, -1).astype(F32)
+        gate_share, up_share = (
+            exchanged(total.reshape(ring, own, hidden_part), mine, ring)
+            .transpose(1, 0, 2)
+            .reshape(own, -1)
+            .astype(F32)
+            for total in (gate_sum, up_sum)
+        )
         output_share = output_share.astype(F32)
     mixer_share, head_share, feedgain_share, bias_share, expand_share, squeeze_share = jnp.split(
         share, cuts

time: 728 us -> 748 us (1.027)
  local copies, waits for them, and re-layouts: 102 us -> 71.8 us
  Pallas kernels: 379 us -> 401 us
  waiting for transfers between devices: 44.3 us -> 62.7 us
  matrix products: 152 us -> 164 us
    pallas_call x1, Pallas kernels: 80.9 us -> 107 us  [start(): pl.pallas_call(functools.partial(start_kernel, ring, lines), out_shape=(j...]
    another operation x3 -> x0, local copies, waits for them, and re-layouts: 16.6 us -> none  [local(): w_gate, w_up = over_batch(feed_columns)]
    reduce_scatter x1, waiting for transfers between devices: 9.27 us -> 21.4 us  [local(): lax.psum_scatter(term_down, 'batch', scatter_dimension=0, tiled=True)]
    unnamed x202 -> x139, local copies, waits for them, and re-layouts: 54.3 us -> 49.3 us
  transfers between devices with their start and end apart: 14 -> 15, of which waited for: 7 -> 5; matrix products, arithmetic and copies ran while one was open for 30% -> 28% of each run, Pallas kernels for 26% -> 25%
where the time goes in v6:
time: 748 us; the launch traced here: 742 us
  Pallas kernels  401 us (54%)
  matrix products  164 us (22%)
  local copies, waits for them, and re-layouts  71.8 us (10%)
  waiting for transfers between devices  62.7 us (8%)
  other arithmetic  17.3 us (2%)
  between operations  15.1 us (2%)
  starting transfers between devices  9.54 us (1%)
    pallas_call x2, Pallas kernels, fold(): pl.pallas_call(functools.partial(fold_kernel, finish, len(given)), out_sh...  151 us
    pallas_call x1, Pallas kernels, finish(): pl.pallas_call(functools.partial(finish_kernel, lines), out_shape=(square...  110 us
    pallas_call x1, Pallas kernels, start(): pl.pallas_call(functools.partial(start_kernel, ring, lines), out_shape=(j...  107 us
    dot_general x8, matrix products, dot_nn(): lax.dot_general(left, right, (((1,), (0,)), ((), ())), preferred_element_...  60.1 us
    dot_general x8, matrix products, dot_nt(): lax.dot_general(left, right, (((1,), (1,)), ((), ())), preferred_element_...  54.5 us
    unnamed x139, local copies, waits for them, and re-layouts  49.3 us
    dot_general x7, matrix products, dot_tn(): lax.dot_general(left, right, (((0,), (0,)), ((), ())), preferred_element_...  49.3 us
    all_gather x1, waiting for transfers between devices, local(): lax.all_gather(after(down_weight, gate_columns), 'batch', axis=0, tiled=T...  22.8 us
  transfers between devices with their start and end apart: 15, of which 5 were waited for; matrix products, arithmetic and copies ran while one was open for 28% of the time, Pallas kernels for 25%

profile of v6, /device:TPU:0, one launch (start us, length us, event | category | flops | bytes accessed | tf_op | source)
XLA Modules:
  0.0 741.7 jit_solution(9815688464731862194)
XLA Ops:
  9.6 2.8 concatenate.39
  20.5 106.9 %start.1 = (bf16[4,256,2048]{2,1,0:T(8,128)(2,1)S(1)}, bf16[4,8,64,1536]{3,2,1,0:T(8,128)(2,1)S(1)}, bf16[4,64,512]{2,1,0:T(8,128)(2,1)}, bf16[8,64,2048]{2,1,0:...) custom-call(bf16[256,2048]{1,0:T(8,128)(2,1)S(1)} %bitcast.112, ...), custom_call_target="tpu_custom_call" | custom-call | tf_op jit(solution)/shard_map/start/pallas_call | solution.py:536
  127.4 1.9 copy-done
  129.4 2.6 copy-done.27
  132.0 1.4 copy-done.31
  135.6 1.5 collective-permute-start.1
  137.1 3.1 fusion
  142.8 3.2 fusion.2
  146.0 2.0 copy-done.34
  148.0 8.9 %convolution_convert_fusion.4.query.key.value = bf16[1024,1536]{1,0:T(8,128)(2,1)S(1)} fusion(bf16[1024,2048]{1,0:T(8,128)(2,1)S(1)} %bitcast.128, bf16[2048,1536]{1,0:T(8,128)(2,1)} %bitcast.116), kind=kOutput, calls=%fused_computation.22 | convolution fusion | flops 6444023808 | bytes 13631488 | tf_op jit(solution)/shard_map/dot_general | solution.py:25
  157.4 3.5 convolution_convert_fusion.9
  162.1 2.5 constant_dynamic-update-slice_fusion.4
  164.6 1.9 slice.77
  166.5 1.4 collective-permute-start.2
  167.9 11.9 %mixer_forward.1 = (f32[1024,512]{1,0:T(8,128)S(1)}, f32[128,1024]{1,0:T(8,128)S(1)}, f32[8,128,512]{2,1,0:T(8,128)S(1)}) custom-call(s32[1]{0:T(128)} %bitcast.mine, bf16[1024,1536]{1,0:T(8,128)(2,1)S(1)} %convolution_convert_fusion.4.query.key.value, bf16[1024,1536]{1,0:T(8,128)(2,1)S(1)} %convolution_convert_fusion.4.query.key.value, ...), custom_call_target="tpu_custom_call" | custom-call | flops 1048576000 | bytes 6291456 | tf_op jit(solution)/shard_map/mixer_forward/pallas_call | solution.py:285
  179.8 1.4 copy-done.5
  181.2 1.4 copy-done.16
  183.4 1.3 slice.78
  185.3 2.4 constant_dynamic-update-slice_fusion.3
  187.7 2.3 constant_dynamic-update-slice_fusion.2
  190.0 1.9 constant_dynamic-update-slice_fusion.1
  191.9 6.4 collective-permute-done.3
  199.4 2.0 copy.51
  201.7 6.6 multiply_convert_fusion.5
  208.4 2.3 convolution_convert_fusion.6
  210.7 73.8 %fold_forward.1 = (bf16[4,256,2048]{2,1,0:T(8,128)(2,1)S(1)}, f32[256,2048]{1,0:T(8,128)S(1)}) custom-call(bf16[4,256,2048]{2,1,0:T(8,128)(2,1)S(1)} %bitcast.114, bf16[256,2048]{1,0:T(8,128)(2,1)S(1)} %bitcast.113, f32[1,2048]{1,0:T(1,128)S(1)} %reshape.384.refs_2_.refs_3_), custom_call_target="tpu_custom_call" | custom-call | tf_op jit(solution)/shard_map/fold_forward/pallas_call | solution.py:964
  284.5 1.3 copy-done.9
  285.8 1.9 copy-done.29
  287.8 11.7 %fusion.23 = f32[1024,1408]{1,0:T(8,128)} fusion(bf16[1024,2048]{1,0:T(8,128)(2,1)} %bitcast.122, bf16[2048,1408]{1,0:T(8,128)(2,1)} %all-gather.7.cloned.1.call-done), kind=kOutput, calls=%fused_computation.92 | convolution fusion | flops 5905580032 | bytes 15728640 | tf_op jit(solution)/shard_map/dot_general | solution.py:25
  299.5 12.9 %multiply_convert_fusion.3 = (bf16[1024,1408]{1,0:T(8,128)(2,1)S(1)}, f32[1024,1408]{1,0:T(8,128)}) fusion(f32[1024,1408]{1,0:T(8,128)} %fusion.23, bf16[1024,2048]{1,0:T(8,128)(2,1)} %bitcast.123, bf16[2048,1408]{1,0:T(8,128)(2,1)} %all-gather.9.cloned.1.call-done), kind=kOutput, calls=%fused_computation.16 | convolution fusion | flops 5914230784 | bytes 24379392 | tf_op jit(solution)/shard_map/dot_general | solution.py:25
  312.3 1.6 copy-done.55
  313.9 8.2 %convolution_convert_fusion.3 = bf16[1408,2048]{1,0:T(8,128)(2,1)} fusion(bf16[1024,1408]{1,0:T(8,128)(2,1)S(1)} %get-tuple-element.157, bf16[1024,2048]{1,0:T(8,128)(2,1)S(1)} %copy-done.47), kind=kOutput, calls=%fused_computation.13 | convolution fusion | flops 5908463616 | bytes 12845056 | tf_op jit(solution)/shard_map/dot_general | solution.py:33
  322.2 22.8 %all-gather.11.cloned.1.call-done = bf16[1408,2048]{1,0:T(8,128)(2,1)} async-done(((bf16[176,2048]{1,0:T(8,128)(2,1)}), bf16[1408,2048]{1,0:T(8,128)(2,1)}) %all-gather.11.cloned.1.call-update) | async-done | bytes 5767184 | tf_op jit(solution)/shard_map/all_gather | solution.py:1170
  345.0 14.6 %multiply_convert_fusion.1 = (bf16[1024,1408]{1,0:T(8,128)(2,1)S(1)}, bf16[1024,1408]{1,0:T(8,128)(2,1)S(1)}) fusion(f32[1024,1408]{1,0:T(8,128)} %fusion.23, f32[1024,1408]{1,0:T(8,128)} %get-tuple-element.158, bf16[1024,2048]{1,0:T(8,128)(2,1)} %constant_dynamic-update-slice_fusion, bf16[1408,2048]{1,0:T(8,128)(2,1)} %all-gather.11.cloned.1.call-done), kind=kOutput, calls=%fused_computation.14 | convolution fusion | flops 5924323328 | bytes 27262976 | tf_op jit(solution)/shard_map/dot_general | solution.py:29
  359.6 9.8 %fusion.24 = f32[1024,2048]{1,0:T(8,128)S(1)} fusion(bf16[1024,1408]{1,0:T(8,128)(2,1)S(1)} %get-tuple-element.125, bf16[2048,1408]{1,0:T(8,128)(2,1)} %all-gather.7.cloned.1.call-done), kind=kOutput, calls=%fused_computation.93 | convolution fusion | flops 5905580032 | bytes 17039360 | tf_op jit(solution)/shard_map/dot_general | solution.py:29
  369.4 11.2 %add_convert_fusion = bf16[1024,2048]{1,0:T(8,128)(2,1)} fusion(f32[1024,2048]{1,0:T(8,128)S(1)} %fusion.24, bf16[1024,1408]{1,0:T(8,128)(2,1)S(1)} %get-tuple-element.124, bf16[2048,1408]{1,0:T(8,128)(2,1)} %all-gather.9.cloned.1.call-done), kind=kOutput, calls=%fused_computation.7 | convolution fusion | flops 5909774336 | bytes 21233664 | tf_op jit(solution)/shard_map/dot_general | solution.py:29
  380.6 8.7 %convolution_convert_fusion.2 = bf16[2048,1408]{1,0:T(8,128)(2,1)} fusion(bf16[1024,2048]{1,0:T(8,128)(2,1)S(1)} %bitcast.125, bf16[1024,1408]{1,0:T(8,128)(2,1)S(1)} %get-tuple-element.125), kind=kOutput, calls=%fused_computation.12 | convolution fusion | flops 5908463616 | bytes 12845056 | tf_op jit(solution)/shard_map/dot_general | solution.py:33
  389.3 21.4 %reduce-scatter.4.cloned.1.call-done = bf16[176,2048]{1,0:T(8,128)(2,1)} async-done(((bf16[1408,2048]{1,0:T(8,128)(2,1)}), bf16[176,2048]{1,0:T(8,128)(2,1)}) %reduce-scatter.4.cloned.1.call-update) | async-done | bytes 720912 | tf_op jit(solution)/shard_map/reduce_scatter | solution.py:1240
  411.4 11.1 %convolution_convert_fusion.1 = bf16[2048,1408]{1,0:T(8,128)(2,1)} fusion(bf16[1024,2048]{1,0:T(8,128)(2,1)} %bitcast.124, bf16[1024,1408]{1,0:T(8,128)(2,1)} %copy-done.56), kind=kOutput, calls=%fused_computation.11 | convolution fusion | flops 5908463616 | bytes 12845056 | tf_op jit(solution)/shard_map/dot_general | solution.py:33
  422.6 11.0 %convolution_convert_fusion.5 = bf16[1024,2048]{1,0:T(8,128)(2,1)} fusion(bf16[1024,1408]{1,0:T(8,128)(2,1)} %copy-done.55, bf16[1408,2048]{1,0:T(8,128)(2,1)} %all-gather.11.cloned.1.call-done), kind=kOutput, calls=%fused_computation.23 | convolution fusion | flops 5907677184 | bytes 12845056 | tf_op jit(solution)/shard_map/dot_general | solution.py:25
  433.6 3.0 fusion.21
  436.7 1.5 collective-permute-start.4
  438.2 1.5 collective-permute-start.6
  439.6 2.2 copy-done.14
  441.9 77.6 %fold_backward.1 = (bf16[4,256,2048]{2,1,0:T(8,128)(2,1)S(1)}, f32[256,2048]{1,0:T(8,128)S(1)}, f32[1,2048]{1,0:T(1,128)S(1)}) custom-call(bf16[4,256,2048]{2,1,0:T(8,128)(2,1)S(1)} %bitcast.115, bf16[256,2048]{1,0:T(8,128)(2,1)} %bitcast.9.refs_1_, f32[256,2048]{1,0:T(8,128)S(1)} %copy-done.10, f32[1,2048]{1,0:T(1,128)S(1)} %reshape.384.refs_2_.refs_3_), custom_call_target="tpu_custom_call" | custom-call | tf_op jit(solution)/shard_map/fold_backward/pallas_call | solution.py:964
  519.5 3.1 multiply_reduce_fusion.1
  522.7 1.7 subtract_convert_fusion
  524.6 21.3 %mixer_backward.1 = (bf16[1024,1536]{1,0:T(8,128)(2,1)S(1)}, f32[64,1024]{1,0:T(8,128)S(1)}) custom-call(s32[1]{0:T(128)} %bitcast.mine, bf16[1024,1536]{1,0:T(8,128)(2,1)S(1)} %convolution_convert_fusion.4.query.key.value, bf16[1024,1536]{1,0:T(8,128)(2,1)S(1)} %convolution_convert_fusion.4.query.key.value, ...), custom_call_target="tpu_custom_call" | custom-call | flops 2097152000 | bytes 10485760 | tf_op jit(solution)/shard_map/mixer_backward/pallas_call | solution.py:310
  546.9 2.4 fusion.26
  549.4 8.8 %fusion.25 = f32[1024,2048]{1,0:T(8,128)} fusion(bf16[1024,1536]{1,0:T(8,128)(2,1)S(1)} %get-tuple-element.72, bf16[2048,1536]{1,0:T(8,128)(2,1)S(1)} %bitcast.119), kind=kOutput, calls=%fused_computation.94 | convolution fusion | flops 6442450944 | bytes 17825792 | tf_op jit(solution)/shard_map/dot_general | solution.py:29
  558.2 12.2 %convolution_convert_fusion = bf16[2048,2048]{1,0:T(8,128)(2,1)} fusion(bf16[1024,512]{1,0:T(8,128)(2,1)S(1)} %get-tuple-element.129, bf16[1024,1536]{1,0:T(8,128)(2,1)S(1)} %get-tuple-element.72, bf16[1024,2048]{1,0:T(8,128)(2,1)S(1)} %bitcast.109, f32[2048]{0:T(1024)S(1)} %copy-done.53, f32[1024]{0:T(1024)S(1)} %bitcast.147), kind=kOutput, calls=%fused_computation.10 | convolution fusion | flops 8610906112 | bytes 16789504 | tf_op jit(solution)/shard_map/dot_general | solution.py:33
  570.4 6.4 multiply_reduce_fusion
  578.8 2.1 add_convert_fusion.3
  581.4 1.8 collective-permute-start.5
  583.2 1.8 fusion.8
  586.5 6.4 convolution_convert_fusion.7
  592.9 9.3 %collective-permute-done.7 = bf16[256,2048]{1,0:T(8,128)(2,1)} collective-permute-done((bf16[256,2048]{1,0:T(8,128)(2,1)S(1)}, bf16[256,2048]{1,0:T(8,128)(2,1)}, u32[]{:S(2)}, u32[]{:S(2)}) %collective-permute-start.7) | collective-permute-done | bytes 1048608 | tf_op jit(solution)/shard_map/ppermute | solution.py:985
  602.2 1.3 collective-permute-done.5
  603.5 3.5 fusion.10
  608.3 109.9 %finish.1 = (f32[64,2048]{1,0:T(8,128)}, f32[64,2048]{1,0:T(8,128)}, f32[64,2048]{1,0:T(8,128)}, f32[64,2048]{1,0:T(8,128)}, f32[64,2048]{1,0:T(8,128)}, /*index...) custom-call(bf16[4,8,64,2048]{3,2,1,0:T(8,128)(2,1)} %bitcast.132, ...), custom_call_target="tpu_custom_call" | custom-call | tf_op jit(solution)/shard_map/finish/pallas_call | solution.py:930
  718.2 1.4 fusion.22
  723.8 2.3 copy.90
  726.1 2.0 copy.91
  728.1 1.9 copy.92
  (212 shorter events, 35.9 us)
Async XLA Ops:
  7.2 192.2 %all-gather.5.cloned.1.call-start = ((), (), s32[]{:S(2)}) async-start(), calls=%async_computation.3 | async-start | bytes 2359296 | tf_op jit(solution)/shard_map/all_gather | solution.py:1158
  127.4 1.9 copy-start
  129.4 2.6 copy-start.27
  132.0 1.4 copy-start.31
  133.4 154.4 %all-gather.7.cloned.1.call-start = ((), (), s32[]{:S(2)}) async-start(), calls=%async_computation.4 | async-start | bytes 6488064 | tf_op jit(solution)/shard_map/all_gather | solution.py:1158
  134.2 165.3 %all-gather.9.cloned.1.call-start = ((), (), s32[]{:S(2)}) async-start(), calls=%async_computation.5 | async-start | bytes 6488064 | tf_op jit(solution)/shard_map/all_gather | solution.py:1158
  134.9 210.1 %all-gather.11.cloned.1.call-start = ((), (), s32[]{:S(2)}) async-start(), calls=%async_computation.6 | async-start | bytes 6488064 | tf_op jit(solution)/shard_map/all_gather | solution.py:1170
  134.9 48.5 %collective-permute-start = (bf16[256,2048]{1,0:T(8,128)(2,1)}, bf16[256,2048]{1,0:T(8,128)(2,1)}, u32[]{:S(2)}, u32[]{:S(2)}) collective-permute-start(bf16[256,2048]{1,0:T(8,128)(2,1)} %bitcast.9.refs_1_), channel_id=1, source_target_pairs={{0,8},{8,0},{16,24},{24,16},{1,9},{9,1},{17,25},{25,17},{2,10},{10... | collective-permute-start | bytes 3145736 | tf_op jit(solution)/shard_map/ppermute | solution.py:985
  135.6 29.0 %collective-permute-start.1 = (bf16[256,2048]{1,0:T(8,128)(2,1)}, bf16[256,2048]{1,0:T(8,128)(2,1)}, u32[]{:S(2)}, u32[]{:S(2)}) collective-permute-start(bf16[256,2048]{1,0:T(8,128)(2,1)} %bitcast.9.refs_1_), channel_id=1, source_target_pairs={{0,16},{8,24},{16,0},{24,8},{1,17},{9,25},{17,1},{25,9},{2,18},{10... | collective-permute-start | bytes 3145736 | tf_op jit(solution)/shard_map/ppermute | solution.py:985
  137.0 273.6 %reduce-scatter.4.cloned.1.call-start = ((), (), s32[]{:S(2)}) async-start(), calls=%async_computation.7 | async-start | bytes 6488064 | tf_op jit(solution)/shard_map/reduce_scatter | solution.py:1240
  141.2 4.8 copy-start.52
  142.6 18.3 %copy-start.51 = (bf16[256,16]{1,0:T(8,128)(2,1)}, bf16[256,16]{1,0:T(8,128)(2,1)S(1)}, u32[]{:S(2)}) copy-start(bf16[256,16]{1,0:T(8,128)(2,1)S(1)} %reshape.349) | copy-start | bytes 24580
  146.0 2.0 copy-start.34
  160.9 7.0 copy-start.49
  162.1 17.7 %copy-start.12 = (f32[128,1024]{1,0:T(8,128)}, f32[128,1024]{1,0:T(8,128)S(1)}, u32[]{:S(2)}) copy-start(f32[128,1024]{1,0:T(8,128)S(1)} %pad_maximum_fusion.2.rate) | copy-start | bytes 1572868
  166.5 23.5 %collective-permute-start.2 = (bf16[128,2048]{1,0:T(8,128)(2,1)}, bf16[128,2048]{1,0:T(8,128)(2,1)}, u32[]{:S(2)}, u32[]{:S(2)}) collective-permute-start(bf16[128,2048]{1,0:T(8,128)(2,1)} %slice.77), channel_id=1, source_target_pairs={{0,8},{8,0},{16,24},{24,16},{1,9},{9,1},{17,25},{25,17},{2,10},{10... | collective-permute-start | bytes 1572872 | tf_op jit(solution)/shard_map/ppermute | solution.py:985
  179.8 1.4 copy-start.5
  181.2 1.4 copy-start.16
  183.4 15.7 %copy-start.6 = (f32[1024,512]{1,0:T(8,128)S(1)}, f32[1024,512]{1,0:T(8,128)}, u32[]{:S(2)}) copy-start(f32[1024,512]{1,0:T(8,128)} %copy-done.5) | copy-start | bytes 6291460
  184.7 13.6 %collective-permute-start.3 = (bf16[128,2048]{1,0:T(8,128)(2,1)S(1)}, bf16[128,2048]{1,0:T(8,128)(2,1)S(1)}, u32[]{:S(2)}, u32[]{:S(2)}) collective-permute-start(bf16[128,2048]{1,0:T(8,128)(2,1)S(1)} %slice.78), channel_id=1, source_target_pairs={{0,16},{8,24},{16,0},{24,8},{1,17},{9,25},{17,1},{25,9},{2,18},{10... | collective-permute-start | bytes 1572872 | tf_op jit(solution)/shard_map/ppermute | solution.py:985
  199.4 2.3 copy-start.7
  201.4 7.0 copy-start.37
  201.7 6.6 copy-start.32
  208.4 2.4 copy-start.54
  208.4 2.4 copy-start.4
  285.8 1.9 copy-start.29
  299.5 14.4 %copy-start.47 = (bf16[1024,2048]{1,0:T(8,128)(2,1)S(1)}, bf16[1024,2048]{1,0:T(8,128)(2,1)}, u32[]{:S(2)}) copy-start(bf16[1024,2048]{1,0:T(8,128)(2,1)} %constant_dynamic-update-slice_fusion) | copy-start | bytes 12582916
  312.3 1.6 copy-start.55
  322.1 286.2 %reduce-scatter.6.cloned.1.call-start = ((), (), s32[]{:S(2)}) async-start(), calls=%async_computation.8 | async-start | bytes 6488064 | tf_op jit(solution)/shard_map/reduce_scatter | solution.py:1243
  359.6 9.8 %copy-start.56 = (bf16[1024,1408]{1,0:T(8,128)(2,1)}, bf16[1024,1408]{1,0:T(8,128)(2,1)S(1)}, u32[]{:S(2)}) copy-start(bf16[1024,1408]{1,0:T(8,128)(2,1)S(1)} %get-tuple-element.124) | copy-start | bytes 8650756
  369.4 11.2 %copy-start.30 = (bf16[4,256,2048]{2,1,0:T(8,128)(2,1)S(1)}, bf16[4,256,2048]{2,1,0:T(8,128)(2,1)}, u32[]{:S(2)}) copy-start(bf16[4,256,2048]{2,1,0:T(8,128)(2,1)} %copy-done.29) | copy-start | bytes 12582916
  410.7 197.6 %reduce-scatter.8.cloned.1.call-start = ((), (), s32[]{:S(2)}) async-start(), calls=%async_computation.9 | async-start | bytes 6488064 | tf_op jit(solution)/shard_map/reduce_scatter | solution.py:1246
  433.6 6.0 copy-start.10
  433.6 85.9 %copy-start.33 = (bf16[8,64,2048]{2,1,0:T(8,128)(2,1)S(1)}, bf16[8,64,2048]{2,1,0:T(8,128)(2,1)}, u32[]{:S(2)}) copy-start(bf16[8,64,2048]{2,1,0:T(8,128)(2,1)} %copy-done.31) | copy-start | bytes 6291460
  436.7 82.8 %copy-start.8 = (f32[1024,512]{1,0:T(8,128)S(1)}, f32[1024,512]{1,0:T(8,128)}, u32[]{:S(2)}) copy-start(f32[1024,512]{1,0:T(8,128)} %copy-done.5) | copy-start | bytes 6291460
  436.7 142.1 %collective-permute-start.4 = (bf16[128,2048]{1,0:T(8,128)(2,1)}, bf16[128,2048]{1,0:T(8,128)(2,1)}, u32[]{:S(2)}, u32[]{:S(2)}) collective-permute-start(bf16[128,2048]{1,0:T(8,128)(2,1)} %get-tuple-element.133), channel_id=1, source_target_pairs={{0,16},{8,24},{16,0},{24,8},{1,17},{9,25},{17,1},{25,9},{2,18},{10... | collective-permute-start | bytes 1572872 | tf_op jit(solution)/shard_map/ppermute | solution.py:985
  438.2 140.6 %collective-permute-start.6 = (bf16[128,2048]{1,0:T(8,128)(2,1)}, bf16[128,2048]{1,0:T(8,128)(2,1)}, u32[]{:S(2)}, u32[]{:S(2)}) collective-permute-start(bf16[128,2048]{1,0:T(8,128)(2,1)} %get-tuple-element.132), channel_id=1, source_target_pairs={{0,8},{8,0},{16,24},{24,16},{1,9},{9,1},{17,25},{25,17},{2,10},{10... | collective-permute-start | bytes 1572872 | tf_op jit(solution)/shard_map/ppermute | solution.py:985
  439.6 2.2 copy-start.14
  441.9 77.7 %copy-start.36 = (f32[1024,512]{1,0:T(8,128)S(1)}, f32[1024,512]{1,0:T(8,128)}, u32[]{:S(2)}) copy-start(f32[1024,512]{1,0:T(8,128)} %get-tuple-element.156) | copy-start | bytes 6291460
  519.5 3.2 copy-start.15
  519.5 3.2 copy-start.28
  522.7 1.8 copy-start.13
  522.7 1.8 copy-start.17
  522.7 1.8 copy-start.21
  522.7 26.6 %slice-start = ((s8[6291456]{0:T(1024)(128)(4,1)}), s8[4194304]{0:T(1024)(128)(4,1)S(1)}, s32[]{:S(2)}) async-start(s8[6291456]{0:T(1024)(128)(4,1)} %bitcast.117), calls=%async_computation.10 | async-start | bytes 8388608
  524.6 21.3 %copy-start.48 = (f32[64,1024]{1,0:T(8,128)S(1)}, f32[64,1024]{1,0:T(8,128)}, u32[]{:S(2)}) copy-start(f32[64,1024]{1,0:T(8,128)} %get-tuple-element.154) | copy-start | bytes 786436
  524.6 22.4 %copy-start.38 = (bf16[4,8,64,512]{3,2,1,0:T(8,128)(2,1)S(1)}, bf16[4,8,64,512]{3,2,1,0:T(8,128)(2,1)}, u32[]{:S(2)}) copy-start(bf16[4,8,64,512]{3,2,1,0:T(8,128)(2,1)} %copy-done.37) | copy-start | bytes 6291460
  524.6 24.8 %slice-start.1 = ((s8[6291456]{0:T(1024)(128)(4,1)}), s8[2097152]{0:T(1024)(128)(4,1)S(1)}, s32[]{:S(2)}) async-start(s8[6291456]{0:T(1024)(128)(4,1)} %bitcast.117), calls=%async_computation.11 | async-start | bytes 4194304
  549.3 8.9 %copy-start.1 = (bf16[4,256,2048]{2,1,0:T(8,128)(2,1)S(1)}, bf16[4,256,2048]{2,1,0:T(8,128)(2,1)}, u32[]{:S(2)}) copy-start(bf16[4,256,2048]{2,1,0:T(8,128)(2,1)} %copy-done) | copy-start | bytes 12582916
  549.4 8.9 %copy-start.53 = (f32[2048]{0:T(1024)S(1)}, f32[2048]{0:T(1024)}, u32[]{:S(2)}) copy-start(f32[2048]{0:T(1024)} %copy-done.52) | copy-start | bytes 24580
  558.2 12.2 %copy-start.35 = (bf16[2048,16]{1,0:T(8,128)(2,1)S(1)}, bf16[2048,16]{1,0:T(8,128)(2,1)}, u32[]{:S(2)}) copy-start(bf16[2048,16]{1,0:T(8,128)(2,1)} %reshape.350) | copy-start | bytes 196612
  570.4 8.0 %copy-start.50 = (bf16[1024,16]{0,1:T(8,128)(2,1)S(1)}, bf16[1024,16]{0,1:T(8,128)(2,1)}, u32[]{:S(2)}) copy-start(bf16[1024,16]{0,1:T(8,128)(2,1)} %copy-done.49) | copy-start | bytes 98308
  570.4 10.4 %copy-start.40 = (bf16[128,2048]{1,0:T(8,128)(2,1)S(1)}, bf16[128,2048]{1,0:T(8,128)(2,1)}, u32[]{:S(2)}) copy-start(bf16[128,2048]{1,0:T(8,128)(2,1)} %get-tuple-element.131) | copy-start | bytes 1572868
  576.9 4.5 copy-start.39
  578.7 4.5 copy-start.2
  580.9 21.2 %collective-permute-start.7 = (bf16[256,2048]{1,0:T(8,128)(2,1)S(1)}, bf16[256,2048]{1,0:T(8,128)(2,1)}, u32[]{:S(2)}, u32[]{:S(2)}) collective-permute-start(bf16[256,2048]{1,0:T(8,128)(2,1)S(1)} %pad_maximum_fusion.1), channel_id=1, source_target_pairs={{0,16},{8,24},{16,0},{24,8},{1,17},{9,25},{17,1},{25,9},{2,18},{10... | collective-permute-start | bytes 3145736 | tf_op jit(solution)/shard_map/ppermute | solution.py:985
  581.4 22.1 %collective-permute-start.5 = (bf16[256,2048]{1,0:T(8,128)(2,1)S(1)}, bf16[256,2048]{1,0:T(8,128)(2,1)}, u32[]{:S(2)}, u32[]{:S(2)}) collective-permute-start(bf16[256,2048]{1,0:T(8,128)(2,1)S(1)} %pad_maximum_fusion), channel_id=1, source_target_pairs={{0,8},{8,0},{16,24},{24,16},{1,9},{9,1},{17,25},{25,17},{2,10},{10... | collective-permute-start | bytes 3145736 | tf_op jit(solution)/shard_map/ppermute | solution.py:985
  586.5 17.0 %copy-start.11 = (f32[256,2048]{1,0:T(8,128)S(1)}, f32[256,2048]{1,0:T(8,128)}, u32[]{:S(2)}) copy-start(f32[256,2048]{1,0:T(8,128)} %copy-done.9) | copy-start | bytes 6291460
  592.9 14.2 %copy-start.43 = (bf16[176,2048]{1,0:T(8,128)(2,1)S(1)}, bf16[176,2048]{1,0:T(8,128)(2,1)}, u32[]{:S(2)}) copy-start(bf16[176,2048]{1,0:T(8,128)(2,1)} %reduce-scatter.4.cloned.1.call-done) | copy-start | bytes 2162692
  718.2 11.8 %copy-start.46 = (f32[64,2048]{1,0:T(8,128)S(1)}, f32[64,2048]{1,0:T(8,128)}, u32[]{:S(2)}) copy-start(f32[64,2048]{1,0:T(8,128)} %get-tuple-element.182) | copy-start | bytes 1572868
  718.2 12.6 %copy-start.45 = (f32[64,2048]{1,0:T(8,128)S(1)}, f32[64,2048]{1,0:T(8,128)}, u32[]{:S(2)}) copy-start(f32[64,2048]{1,0:T(8,128)} %get-tuple-element.186) | copy-start | bytes 1572868
  718.2 13.4 %copy-start.44 = (f32[64,2048]{1,0:T(8,128)S(1)}, f32[64,2048]{1,0:T(8,128)}, u32[]{:S(2)}) copy-start(f32[64,2048]{1,0:T(8,128)} %get-tuple-element.188) | copy-start | bytes 1572868
  718.2 14.2 %copy-start.42 = (f32[64,5632]{1,0:T(8,128)S(1)}, f32[64,5632]{1,0:T(8,128)}, u32[]{:S(2)}) copy-start(f32[64,5632]{1,0:T(8,128)} %get-tuple-element.190) | copy-start | bytes 4325380
  726.1 7.4 copy-start.41
  (10 other events, 10.3 us)
Sparse Core Ops, SparseCore 0:
  133.5 28.3 all-gather.4
  163.5 59.9 all-gather.6
  225.2 59.1 all-gather.8
  285.8 59.1 all-gather.10
  347.1 63.5 reduce-scatter.3
  412.8 63.2 reduce-scatter.5
  478.4 63.2 reduce-scatter.7

commit v7 on v6

--- a/solution.py
+++ b/solution.py
@@ -279,8 +279,8 @@
     return count, wide, everything, pair, slim, rows, state
 
 
-def mixer_forward(mine, ring, joined, rates, rows):
-    length, size = joined.shape[0], joined.shape[1] // 3
+def mixer_forward(mine, ring, size, joined, rates, rows):
+    length = joined.shape[0]
     count, wide, _, pair, _, row_spec, state = mixer_specs(length, size, ring, False)
     return pl.pallas_call(
         functools.partial(mixer_forward_kernel, size ** (-0.25)),
@@ -378,190 +378,6 @@
                 pl.when(when)(copy.wait_send)
 
 
-def slab_chain(copies, chips, place):
-    mine, batch = lax.axis_index("seq"), lax.axis_index("batch")
-    chip, core = batch // 2, batch % 2
-    other = (mine, chip * 2 + (1 - core))
-
-    def at(where):
-        return jnp.clip(where, 0, chips - 1) * 2 + core
-
-    def send(step, way):
-        block, come = chip - way * (step - 1), chip - way * step
-        when = (block >= 0) & (block < chips) & (chip + way >= 0) & (chip + way < chips)
-        came = (come >= 0) & (come < chips)
-        wait = copies.far(
-            place(at(block)), place(at(block)), place(at(come)), (mine, at(chip + way)), when
-        )
-        return wait, came, at(come)
-
-    crossing = [(copies.far(place(batch), place(batch), place(other[1]), other), None)]
-    flying = [send(1, 1), send(1, -1)] if chips > 1 else []
-    yield
-    for step in range(1, chips):
-        coming = []
-        for way, (wait, came, landed) in zip((1, -1), flying):
-            pl.when(came)(wait)
-            if step + 1 < chips:
-                coming.append(send(step + 1, way))
-            there = landed + 1 - 2 * core
-            crossing.append(
-                (copies.far(place(landed), place(landed), place(there), other, came), came)
-            )
-        flying = coming
-        yield
-    for wait, came in crossing:
-        if came is None:
-            wait()
-        else:
-            pl.when(came)(wait)
-    yield
-
-
-def start_kernel(
-    ring, lines, inputs, w_query, w_key, w_value, w_swish, w_out, gate, up, small,
-    inputs_all, w_mixer, swish_columns, w_output, gate_columns, up_columns, small_all,
-    own_input, mixer_blocks, swish_blocks, own_out, gate_blocks, up_blocks,
-    local_sem, send_sem, recv_sem,
-):
-    mine, batch = lax.axis_index("seq"), lax.axis_index("batch")
-    chips = lines // 2
-    copies = Copies(local_sem, send_sem, recv_sem)
-    part = swish_columns.shape[2]
-    half = inputs.shape[0] // 2
-    others = peers(ring, mine)
-
-    def columns(ref, blocks, first, size):
-        return [
-            copies.near(
-                ref.at[at] if len(ref.shape) == 3 else ref.at[:, pl.ds(at * size, size)],
-                blocks.at[at, :, pl.ds(first, size)],
-            )
-            for at in range(ring)
-        ]
-
-    loads = []
-    for at, ref in enumerate((w_query, w_key, w_value)):
-        loads += columns(ref, mixer_blocks, at * part, part)
-    direct = 2 if ring == 4 else ring - 1
-    input_waits = [
-        copies.far(inputs, inputs_all.at[by + 1], inputs_all.at[by + 1], (others[by], batch))
-        for by in range(direct)
-    ]
-    own_load = copies.near(inputs, own_input)
-    hidden = gate_columns.shape[2]
-    out_load = copies.near(w_out, own_out)
-    other_loads = columns(w_swish, swish_blocks, 0, part)
-    other_loads += columns(gate, gate_blocks, 0, hidden) + columns(up, up_blocks, 0, hidden)
-    for copy in loads:
-        copy.wait()
-    column_waits = [
-        copies.far(
-            mixer_blocks.at[to], w_mixer.at[mine, batch], w_mixer.at[to, batch], (to, batch)
-        )
-        for to in others
-    ]
-    near = [
-        copies.near(mixer_blocks.at[mine], w_mixer.at[mine, batch]),
-        copies.near(small, small_all.at[mine, batch]),
-    ]
-    small_waits = [
-        copies.far(small, small_all.at[mine, batch], small_all.at[to, batch], (to, batch))
-        for to in others
-    ]
-    for copy in near:
-        copy.wait()
-
-    def started(place):
-        chain = slab_chain(copies, chips, place)
-        next(chain)
-        chains.append(chain)
-
-    chains = []
-    started(lambda at: w_mixer.at[mine, at])
-    for wait, source in zip(column_waits, others):
-        wait()
-        started(lambda at, source=source: w_mixer.at[source, at])
-    for wait, source in zip(small_waits, others):
-        wait()
-        started(lambda at, source=source: small_all.at[source, at])
-    started(lambda at: small_all.at[mine, at])
-    out_load.wait()
-    near = copies.near(own_out, w_output.at[batch])
-    near.wait()
-    started(lambda at: w_output.at[at])
-    own_load.wait()
-    stores = [copies.near(own_input, inputs_all.at[0])]
-    for copy in other_loads:
-        copy.wait()
-    moved = (
-        (swish_blocks, swish_columns), (gate_blocks, gate_columns), (up_blocks, up_columns)
-    )
-    stores += [copies.near(blocks.at[mine], array.at[mine]) for blocks, array in moved]
-    for wait in input_waits:
-        wait()
-    if ring == 4:
-        low, high = pl.ds(0, half), pl.ds(half, half)
-        input_waits = [
-            copies.far(
-                inputs_all.at[have, rows], inputs_all.at[3, rows], inputs_all.at[3, rows], (to, batch)
-            )
-            for have, rows, to in ((2, low, others[0]), (1, high, others[1]))
-        ]
-    else:
-        input_waits = []
-    other_waits = [
-        copies.far(blocks.at[to], array.at[mine], array.at[to], (to, batch))
-        for blocks, array in moved
-        for to in others
-    ]
-    for step in range(1, chips + 1):
-        for chain in chains:
-            next(chain)
-    for wait in input_waits + other_waits:
-        wait()
-    for copy in stores:
-        copy.wait()
-    copies.close()
-
-
-def start(ring, lines, inputs, columns, w_out, gate, up, small):
-    own, width = columns[0].shape
-    part, hidden = width // ring, gate.shape[1] // ring
-    if hidden % 128:
-        gate, up = (a.reshape(own, ring, hidden).transpose(1, 0, 2) for a in (gate, up))
-    anywhere, outside = (pl.BlockSpec(memory_space=space) for space in (pl.ANY, pltpu.HBM))
-    away = (ring - 1) * 6 + 2 + (2 * ring + 1) * (4 * (lines // 2 - 1) + 1)
-    thin = (ring, own, hidden)
-    return pl.pallas_call(
-        functools.partial(start_kernel, ring, lines),
-        out_shape=(
-            jax.ShapeDtypeStruct((ring,) + inputs.shape, BF16),
-            jax.ShapeDtypeStruct((ring, lines, own, 3 * part), BF16),
-            jax.ShapeDtypeStruct((ring, own, part), BF16),
-            jax.ShapeDtypeStruct((lines,) + w_out.shape, BF16),
-            jax.ShapeDtypeStruct(thin, BF16),
-            jax.ShapeDtypeStruct(thin, BF16),
-            jax.ShapeDtypeStruct((ring, lines) + small.shape, BF16),
-        ),
-        in_specs=[anywhere] * 9,
-        out_specs=[outside] * 7,
-        scratch_shapes=[
-            pltpu.VMEM(inputs.shape, BF16),
-            pltpu.VMEM((ring, own, 3 * part), BF16),
-            pltpu.VMEM((ring, own, part), BF16),
-            pltpu.VMEM(w_out.shape, BF16),
-            pltpu.VMEM(thin, BF16),
-            pltpu.VMEM(thin, BF16),
-            pltpu.SemaphoreType.DMA((6 * ring + 9,)),
-            pltpu.SemaphoreType.DMA((away,)),
-            pltpu.SemaphoreType.DMA((away,)),
-        ],
-        compiler_params=pltpu.CompilerParams(has_side_effects=True, vmem_limit_bytes=32 << 20),
-        name="start",
-    )(inputs, *columns, w_out, gate, up, small)
-
-
 PARTS = 4
 
 
@@ -696,265 +512,6 @@
     )
     made[0][full, :] = grad
     return grad.astype(BF16)
-
-
-def finish_kernel(
-    lines, mixer_terms, out_terms, input_terms, gate_sum, up_sum, small_terms, inputs, gain, grad_hidden,
-    grad_query, grad_key, grad_value, grad_swish, grad_out, grad_gate, grad_up, grad_input, small_sum,
-    crossed, staged, arrived, summed, outgoing, mixer_blocks, feed_blocks, small_ring, small_mine, small_line,
-    first, second, third, two_low, one_high, local_sem, send_sem, recv_sem,
-):
-    mine, batch = lax.axis_index("seq"), lax.axis_index("batch")
-    chips = lines // 2
-    chip, core = batch // 2, batch % 2
-    sibling = chip * 2 + (1 - core)
-    others = peers(4, mine)
-    row, col = (others[0], batch), (others[1], batch)
-    copies = Copies(local_sem, send_sem, recv_sem)
-    slabs = others + [mine, None]
-
-    def term(slab, owner):
-        return out_terms.at[owner] if slabs[slab] is None else mixer_terms.at[slabs[slab], owner]
-
-    cross_waits = {}
-    for slab in range(len(slabs)):
-        for owner in range(chips):
-            cross_waits[slab, owner] = copies.far(
-                term(slab, owner * 2 + (1 - core)),
-                crossed.at[slab, owner],
-                crossed.at[slab, owner],
-                (mine, sibling),
-            )
-    small_waits = [
-        copies.far(small_terms.at[to], small_ring.at[at], small_ring.at[at], (to, batch))
-        for at, to in enumerate(others)
-    ]
-    feed_waits = [
-        copies.far(
-            array.at[to], feed_blocks.at[mine, at], feed_blocks.at[to, at], (to, batch)
-        )
-        for to in others
-        for at, array in enumerate((gate_sum, up_sum))
-    ]
-
-    size = input_terms.shape[1] // PARTS
-    opening, direct = [], []
-
-    def span(at):
-        low = pl.ds(at * size, size // 2)
-        return pl.ds(at * size, size), low, pl.ds(at * size + size // 2, size // 2)
-
-    def open_part(at):
-        _, low, high = span(at)
-        opening.append(
-            (
-                copies.far(input_terms.at[3, low], first.at[low], first.at[low], row),
-                copies.far(input_terms.at[3, high], first.at[high], first.at[high], col),
-            )
-        )
-
-    def pass_part(at):
-        _, low, high = span(at)
-        waits = [
-            copies.far(input_terms.at[2, high], second.at[high], second.at[high], col),
-            copies.far(input_terms.at[1, low], third.at[low], third.at[low], row),
-        ]
-        opening[at][0]()
-        two_low[low, :] = added(input_terms[2, low, :], first[low, :])
-        waits.append(copies.far(two_low.at[low], second.at[low], second.at[low], col))
-        opening[at][1]()
-        one_high[high, :] = added(input_terms[1, high, :], first[high, :])
-        waits.append(copies.far(one_high.at[high], third.at[high], third.at[high], row))
-        direct.append(waits)
-
-    def close_part(at):
-        full, _, _ = span(at)
-        for wait in direct[at]:
-            wait()
-        total = (
-            input_terms[0, full, :].astype(F32)
-            + second[full, :].astype(F32)
-            + third[full, :].astype(F32)
-        )
-        features = inputs[full, :].astype(F32)
-        scale = rms_scale(features)
-        plain = features * scale
-        scaled = total * gain[...]
-        grad = (
-            grad_hidden[full, :]
-            + scale * scaled
-            - plain * (scale * jnp.mean(scaled * plain, axis=-1, keepdims=True))
-        )
-        grad_input[full, :] = grad.astype(BF16)
-
-    def small_part():
-        for wait in small_waits:
-            wait()
-        small_mine[...] = small_terms[mine] + small_ring[0] + small_ring[1] + small_ring[2]
-        for by in range(1, lines):
-            to, source = (batch + by) % lines, (batch + lines - by) % lines
-            small_waits.append(
-                copies.far(small_mine.at[to], small_line.at[by], small_line.at[by], (mine, to))
-            )
-
-    def feed_part():
-        for wait in feed_waits:
-            wait()
-        feed_blocks[mine, 0] = gate_sum[mine]
-        feed_blocks[mine, 1] = up_sum[mine]
-        wide = gate_sum.shape[2]
-        for source in range(4):
-            at = pl.ds(source * wide, wide)
-            grad_gate[:, at] = feed_blocks[source, 0].astype(F32)
-            grad_up[:, at] = feed_blocks[source, 1].astype(F32)
-
-    beside = [functools.partial(open_part, 1)]
-    for at in range(PARTS):
-        if at + 2 <= PARTS - 1:
-            beside.append(functools.partial(open_part, at + 2))
-        beside.append(functools.partial(pass_part, at))
-        if at == 0:
-            beside.append(small_part)
-        if at:
-            beside.append(functools.partial(close_part, at - 1))
-    beside.append(functools.partial(close_part, PARTS - 1))
-    beside.append(feed_part)
-    open_part(0)
-
-    def both_cores(slab, owner):
-        return term(slab, owner * 2 + core)[...].astype(F32) + crossed[slab, owner].astype(F32)
-
-    crossed_in = set()
-
-    def wait_cross(slab):
-        if slab not in crossed_in:
-            crossed_in.add(slab)
-            for owner in range(chips):
-                cross_waits[slab, owner]()
-
-    flying = {}
-    for far in range(chips - 1, 0, -1):
-        for slab in range(len(slabs)):
-            wait_cross(slab)
-            for side, way in enumerate((1, -1)):
-                owner = chip + way * far
-                sends = (owner >= 0) & (owner < chips)
-                held = jnp.clip(owner, 0, chips - 1)
-                before = chip - way
-                gets = sends & (before >= 0) & (before < chips)
-                here = staged.at[side, far - 1, slab]
-                if far < chips - 1:
-                    wait = flying[side, far + 1, slab]
-
-                    @pl.when(gets)
-                    def _(wait=wait, slab=slab, held=held, here=here, side=side, far=far):
-                        wait()
-                        here[...] = (
-                            both_cores(slab, held) + arrived[side, far, slab].astype(F32)
-                        ).astype(BF16)
-
-                    @pl.when(sends & jnp.logical_not((before >= 0) & (before < chips)))
-                    def _(slab=slab, held=held, here=here):
-                        here[...] = both_cores(slab, held).astype(BF16)
-                else:
-
-                    @pl.when(sends)
-                    def _(slab=slab, held=held, here=here):
-                        here[...] = both_cores(slab, held).astype(BF16)
-
-                target = jnp.clip(chip + way, 0, chips - 1) * 2 + core
-                flying[side, far, slab] = copies.far(
-                    here,
-                    arrived.at[side, far - 1, slab],
-                    arrived.at[side, far - 1, slab],
-                    (mine, target),
-                    sends,
-                )
-            if beside:
-                beside.pop(0)()
-    ring_waits = []
-    for slab in range(len(slabs)):
-        total = summed.at[slab]
-        total[...] = both_cores(slab, chip)
-        for side, way in enumerate((1, -1)):
-            before = chip - way
-            wait = flying[side, 1, slab]
-
-            @pl.when((before >= 0) & (before < chips))
-            def _(wait=wait, total=total, slab=slab, side=side):
-                wait()
-                total[...] += arrived[side, 0, slab].astype(F32)
-
-        if slabs[slab] is None:
-            grad_out[...] = total[...]
-        elif slab == len(others):
-            mixer_blocks[mine] = total[...].astype(BF16)
-        else:
-            outgoing[slab] = total[...].astype(BF16)
-            to = slabs[slab]
-            ring_waits.append(
-                copies.far(
-                    outgoing.at[slab], mixer_blocks.at[mine], mixer_blocks.at[to], (to, batch)
-                )
-            )
-        if beside:
-            beside.pop(0)()
-    for piece in beside:
-        piece()
-    for wait in small_waits[3:]:
-        wait()
-    total = small_mine[batch]
-    for by in range(1, lines):
-        total = total + small_line[by]
-    small_sum[...] = total
-    for wait in ring_waits:
-        wait()
-    part = grad_query.shape[1] // 4
-    for source in range(4):
-        at = pl.ds(source * part, part)
-        for piece, out in enumerate((grad_query, grad_key, grad_value, grad_swish)):
-            out[:, at] = mixer_blocks[source, :, piece * part : (piece + 1) * part].astype(F32)
-    copies.close()
-
-
-def finish(lines, mixer_terms, out_terms, input_terms, gate_sum, up_sum, small_terms, inputs, gain, grad_hidden):
-    ring, _, own, width = mixer_terms.shape
-    rows, hidden = inputs.shape[0], gate_sum.shape[2]
-    chips = lines // 2
-    inside = pl.BlockSpec(memory_space=pltpu.VMEM)
-    block = pltpu.VMEM((rows, width), BF16)
-    small = small_terms.shape[2:]
-    away = (ring + 1) * (chips + 2 * (chips - 1)) + 4 * (ring - 1) + PARTS * 6 + lines - 1
-    square = jax.ShapeDtypeStruct((own, width), F32)
-    wide = jax.ShapeDtypeStruct((own, ring * hidden), F32)
-    return pl.pallas_call(
-        functools.partial(finish_kernel, lines),
-        out_shape=(square,) * 5
-        + (wide,) * 2
-        + (jax.ShapeDtypeStruct((rows, width), BF16), jax.ShapeDtypeStruct(small, F32)),
-        in_specs=[inside] * 9,
-        out_specs=[inside] * 9,
-        scratch_shapes=[
-            pltpu.VMEM((ring + 1, chips, own, width), BF16),
-            pltpu.VMEM((2, chips - 1, ring + 1, own, width), BF16),
-            pltpu.VMEM((2, chips - 1, ring + 1, own, width), BF16),
-            pltpu.VMEM((ring + 1, own, width), F32),
-            pltpu.VMEM((ring - 1, own, width), BF16),
-            pltpu.VMEM((ring, own, width), BF16),
-            pltpu.VMEM((ring, 2, own, hidden), BF16),
-            pltpu.VMEM((ring - 1, lines) + small, F32),
-            pltpu.VMEM((lines,) + small, F32),
-            pltpu.VMEM((lines,) + small, F32),
-        ]
-        + [block] * 5
-        + [
-            pltpu.SemaphoreType.DMA((1,)),
-            pltpu.SemaphoreType.DMA((away,)),
-            pltpu.SemaphoreType.DMA((away,)),
-        ],
-        compiler_params=pltpu.CompilerParams(has_side_effects=True, vmem_limit_bytes=58 << 20),
-        name="finish",
-    )(mixer_terms, out_terms, input_terms, gate_sum, up_sum, small_terms, inputs, gain, grad_hidden)
 
 
 def fold(finish, terms, given, made, name):
@@ -1118,22 +675,40 @@
     )
     count = params.shape[0]
     params = jnp.concatenate([params, segments.reshape(rows).astype(BF16)])
-    params = jnp.pad(params, (0, -params.shape[0] % 2048)).reshape(-1, 128)
     input_own = layer_input.reshape(rows, width)
     grad_own = cotangent.reshape(rows, width)
-    inputs, w_mixer, swish_columns, w_output, gate_columns, up_columns, small = start(
-        ring,
-        lines,
-        input_own,
-        (query_weight, key_weight, value_weight, swish_weight),
-        output_weight,
-        gate_weight,
-        up_weight,
-        params,
-    )
-    inputs = inputs.reshape(length, width)
+
+    def permuted(array):
+        shape = array.shape[:-1]
+        array = array.reshape(shape + (ring, lines, own))
+        return jnp.swapaxes(array, -3, -2).reshape(shape + (width,))
+
+    def restored(array):
+        shape = array.shape[:-1]
+        array = array.reshape(shape + (lines, ring, own))
+        return jnp.swapaxes(array, -3, -2).reshape(shape + (width,))
+
+    def columns(*arrays):
+        blocks = [a.reshape(own, ring, a.shape[1] // ring) for a in arrays]
+        return jnp.concatenate(blocks, axis=2).transpose(1, 0, 2)
+
+    w_output = lax.all_gather(output_weight, "batch", axis=0, tiled=True)
+    mixer_columns = exchanged(
+        columns(query_weight, key_weight, value_weight, swish_weight), mine, ring
+    )
+    w_mixer = lax.all_gather(mixer_columns.reshape(ring * own, -1), "batch", axis=0, tiled=True)
+    feed_columns = exchanged(columns(gate_weight, up_weight), mine, ring)
+    w_feed = lax.all_gather(feed_columns.reshape(ring * own, -1), "batch", axis=0, tiled=True)
+    w_down = lax.all_gather(after(down_weight, feed_columns), "batch", axis=0, tiled=True)
+    if ring != 4:
+        w_feed = w_feed.reshape(lines, ring, own, -1).transpose(1, 0, 2, 3).reshape(width, -1)
+
+    def line_major(term):
+        return term.reshape(ring, lines, own, -1).transpose(1, 0, 2, 3).reshape(width, -1)
+
+    inputs = after(gathered(permuted(input_own), ring), w_output)
+    small = doubled(doubled(params[None], "batch"), "seq")
     grad_out = gathered(after(grad_own, inputs), ring)
-    w_mixer = w_mixer.reshape(width, 3 * part)
     small = small.reshape(devices, -1)
     segment = lax.dynamic_index_in_dim(
         small.reshape(ring, lines, -1), lax.axis_index("batch"), 1, keepdims=False
@@ -1142,7 +717,7 @@
     gain_one, gain_head, gain_two, bias_full, expand_t, w_squeeze = jnp.split(
         small[:, :count], cuts, axis=1
     )
-    gain_one = gain_one.reshape(width).astype(F32)
+    gain_one = permuted(gain_one.reshape(width)).astype(F32)
     gain_head = lax.dynamic_slice_in_dim(gain_head.reshape(width), head * head_size, head_size, 0)
     gain_head = gain_head.astype(F32)
     gain_two = gain_two.reshape(width).astype(F32)
@@ -1150,24 +725,7 @@
     expand_head = lax.dynamic_slice_in_dim(
         expand_t.reshape(slots_all, RANK), head * SLOTS, SLOTS, 0
     )
-    w_squeeze = w_squeeze.reshape(width, RANK).T
-
-    w_output = w_output.reshape(part, width)
-
-    def over_batch(blocks):
-        return lax.all_gather(blocks.reshape(ring * own, -1), "batch", axis=0, tiled=True)
-
-    def own_order(array):
-        return array.reshape(lines, ring, own, -1).transpose(1, 0, 2, 3).reshape(width, -1)
-
-    def line_major(term):
-        return term.reshape(ring, lines, own, -1).transpose(1, 0, 2, 3).reshape(width, -1)
-
-    w_swish = own_order(over_batch(swish_columns))
-    w_gate, w_up = over_batch(gate_columns), over_batch(up_columns)
-    if ring != 4:
-        w_gate, w_up = own_order(w_gate), own_order(w_up)
-    w_down = lax.all_gather(after(down_weight, gate_columns), "batch", axis=0, tiled=True)
+    w_squeeze = permuted(w_squeeze.reshape(width, RANK).T)
 
     chunked = segment.reshape(-1, CHUNK)
     before = jnp.concatenate([jnp.full((1,), -1.0, F32), chunked[:-1, -1]])
@@ -1192,13 +750,13 @@
         joined = jnp.concatenate(
             [whole_head(joined[:, at * part : (at + 1) * part]) for at in range(3)], axis=1
         )
-    swish_pre = whole_head(dot_nn(normed, w_swish))
+    swish_pre = whole_head(mixer_pre[:, 3 * part :])
     reduced = dot_nt(normed, w_squeeze).astype(BF16)
     forget_logit = dot_nt(expand_head, reduced) + bias_head.astype(F32)[:, None]
     log_rate = jax.nn.log_sigmoid(forget_logit) / TAU_GATE
     rates = jnp.concatenate([log_rate, -jnp.expm1(log_rate)], axis=0)
     order = mine.reshape(1).astype(jnp.int32)
-    mixed, choice, starts = mixer_forward(order, ring, joined, rates, mask_rows)
+    mixed, choice, starts = mixer_forward(order, ring, head_size, joined, rates, mask_rows)
     mixed, grad_out = lax.optimization_barrier((mixed, grad_out))
     head_factor = rms_scale(mixed)
     head_plain = mixed * head_factor
@@ -1220,7 +778,8 @@
         hidden = input_own.astype(F32) + scattered(terms, ring)
         feed_in = gathered((hidden * rms_scale(hidden) * gain_two).astype(BF16), ring)
 
-    gate_pre, up_pre = dot_nn(feed_in, w_gate), dot_nn(feed_in, w_up)
+    feed_pre = dot_nn(feed_in, w_feed)
+    gate_pre, up_pre = feed_pre[:, :hidden_part], feed_pre[:, hidden_part:]
     gate_sig = jax.nn.sigmoid(gate_pre)
     gate_act = gate_pre * gate_sig
     inner = (gate_act * up_pre).astype(BF16)
@@ -1228,28 +787,23 @@
     term_down = dot_tn(inner, grad_out).astype(BF16)
     grad_inner = dot_nt(after(grad_out, term_down), w_down)
     grad_gatepre = grad_inner * up_pre * (gate_sig * (1.0 + gate_pre * (1.0 - gate_sig)))
-    grad_gatepre = grad_gatepre.astype(BF16)
-    grad_uppre = (grad_inner * gate_act).astype(BF16)
-    back_feedin = (dot_nt(grad_gatepre, w_gate) + dot_nt(grad_uppre, w_up)).astype(BF16)
-    feed_rows = after(feed_in, back_feedin)
-    term_gate = dot_tn(feed_rows, grad_gatepre).astype(BF16)
-    term_up = dot_tn(feed_rows, grad_uppre).astype(BF16)
+    grad_feedpre = jnp.concatenate(
+        [grad_gatepre.astype(BF16), (grad_inner * gate_act).astype(BF16)], axis=1
+    )
+    back_feedin = dot_nt(grad_feedpre, w_feed).astype(BF16)
+    term_feedpre = dot_tn(after(feed_in, back_feedin), grad_feedpre).astype(BF16)
     result_terms = dot_nn(inner, w_down).astype(BF16)
     result = hidden + scattered(result_terms, ring)
     layer_output = result.astype(BF16).reshape(1, rows, width)
     down_share = lax.psum_scatter(term_down, "batch", scatter_dimension=0, tiled=True)
-    if ring != 4:
-        term_gate, term_up = line_major(term_gate), line_major(term_up)
-    gate_sum = lax.psum_scatter(
-        after(term_gate, down_share), "batch", scatter_dimension=0, tiled=True
-    )
-    up_sum = lax.psum_scatter(
-        after(term_up, down_share), "batch", scatter_dimension=0, tiled=True
+    feed_terms = term_feedpre if ring == 4 else line_major(term_feedpre)
+    feed_sum = lax.psum_scatter(
+        after(feed_terms, down_share), "batch", scatter_dimension=0, tiled=True
     )
     if ring == 4:
         grad_branch, grad_hidden, term_feed = fold(
             finish_backward,
-            after(back_feedin, term_gate, term_up).reshape(ring, rows, width),
+            after(back_feedin, term_feedpre).reshape(ring, rows, width),
             (grad_own, hidden, gain_two[None]),
             (
                 jax.ShapeDtypeStruct((rows, width), F32),
@@ -1292,12 +846,31 @@
         grad_pre = jnp.concatenate(
             [own_part(grad_pre[:, at * head_size : (at + 1) * head_size]) for at in range(3)], axis=1
         )
-    grad_normed = (
-        dot_nt(grad_pre, w_mixer) + dot_nt(grad_swishpre, w_swish) + dot_nn(grad_reduced, w_squeeze)
-    )
-    term_pre = dot_tn(normed, jnp.concatenate([grad_pre, grad_swishpre], axis=1)).astype(BF16)
-    term_mixer = (jnp.sum(grad_normed * plain_one, axis=0))
-    term_squeeze = (dot_tn(grad_reduced, normed))
+    grad_pre = jnp.concatenate([grad_pre, grad_swishpre], axis=1)
+    term_pre = dot_tn(normed, grad_pre).astype(BF16)
+    pre_sum = lax.psum_scatter(after(term_pre, feed_sum), "batch", scatter_dimension=0, tiled=True)
+    output_share = lax.psum_scatter(
+        after(term_output, pre_sum), "batch", scatter_dimension=0, tiled=True
+    )
+    grad_normed = dot_nt(grad_pre, w_mixer) + dot_nn(grad_reduced, w_squeeze)
+    term_mixer = restored(jnp.sum(grad_normed * plain_one, axis=0))
+    term_squeeze = restored(dot_tn(grad_reduced, normed))
+    grad_normed = restored(scattered(grad_normed.astype(BF16), ring))
+    inputs_own = input_own.astype(F32)
+    scale_own = rms_scale(inputs_own)
+    scaled_one = grad_normed * restored(gain_one)
+    grad_input = (
+        grad_hidden
+        + scale_own * scaled_one
+        - inputs_own * scale_own**3 * jnp.mean(scaled_one * inputs_own, axis=-1, keepdims=True)
+    ).astype(BF16)
+    pre_share = exchanged(pre_sum.reshape(ring, own, 4 * part), mine, ring)
+    pre_share = pre_share.reshape(ring, own, 4, part).transpose(2, 1, 0, 3)
+    query_share, key_share, value_share, swish_share = pre_share.reshape(4, own, width).astype(F32)
+    feed_share = exchanged(feed_sum.reshape(ring, own, 2 * hidden_part), mine, ring)
+    gate_share = feed_share[:, :, :hidden_part].transpose(1, 0, 2).reshape(own, -1).astype(F32)
+    up_share = feed_share[:, :, hidden_part:].transpose(1, 0, 2).reshape(own, -1).astype(F32)
+
     def placed(array, size):
         full = jnp.zeros((HEADS, size) + array.shape[1:], F32)
         return lax.dynamic_update_slice_in_dim(full, array[None], head, 0)
@@ -1313,47 +886,7 @@
         ],
         axis=1,
     )
-    inputs_own = input_own.astype(F32)
-    if ring == 4:
-        padded = jnp.pad(terms, ((0, 0), (0, -terms.shape[1] % 1024)))
-        outs = finish(
-            lines,
-            term_pre.reshape(ring, lines, own, width),
-            term_output.reshape(lines, own, width),
-            after(grad_normed.astype(BF16), layer_output).reshape(ring, rows, width),
-            gate_sum.reshape(ring, own, hidden_part),
-            up_sum.reshape(ring, own, hidden_part),
-            padded.reshape(ring, lines, -1, 128),
-            input_own,
-            gain_one[None],
-            grad_hidden,
-        )
-        query_share, key_share, value_share, swish_share, output_share, gate_share, up_share = outs[:7]
-        grad_input, share = outs[7], outs[8].reshape(-1)[: terms.shape[1]]
-    else:
-        share = halved(halved(terms, "seq"), "batch")[0]
-        grad_normed = scattered(grad_normed.astype(BF16), ring)
-        scale_own = rms_scale(inputs_own)
-        scaled_one = grad_normed * gain_one
-        grad_input = (
-            grad_hidden
-            + scale_own * scaled_one
-            - inputs_own * scale_own**3 * jnp.mean(scaled_one * inputs_own, axis=-1, keepdims=True)
-        ).astype(BF16)
-        output_share = lax.psum_scatter(term_output, "batch", scatter_dimension=0, tiled=True)
-        pre_sum = lax.psum_scatter(line_major(term_pre), "batch", scatter_dimension=0, tiled=True)
-        pre_share = exchanged(pre_sum.reshape(ring, own, 4 * part), mine, ring)
-        pre_share = pre_share.reshape(ring, own, 4, part).transpose(2, 1, 0, 3)
-        pre_share = pre_share.reshape(4, own, width).astype(F32)
-        query_share, key_share, value_share, swish_share = pre_share
-        gate_share, up_share = (
-            exchanged(total.reshape(ring, own, hidden_part), mine, ring)
-            .transpose(1, 0, 2)
-            .reshape(own, -1)
-            .astype(F32)
-            for total in (gate_sum, up_sum)
-        )
-        output_share = output_share.astype(F32)
+    share = halved(halved(terms, "seq"), "batch")[0]
     mixer_share, head_share, feedgain_share, bias_share, expand_share, squeeze_share = jnp.split(
         share, cuts
     )
@@ -1369,7 +902,7 @@
         bias_share,
         swish_share,
         head_share,
-        output_share,
+        output_share.astype(F32),
         feedgain_share,
         gate_share,
         up_share,

time: 748 us -> 671 us (0.90)
  Pallas kernels: 401 us -> 188 us
  waiting for transfers between devices: 62.7 us -> 146 us
  starting transfers between devices: 9.54 us -> 47.1 us
  other arithmetic: 17.3 us -> 37 us
  matrix products: 164 us -> 149 us
    pallas_call x2 -> x0, Pallas kernels: 217 us -> none  [the longest x1 110 us: finish(): pl.pallas_call(functools.partial(finish_kernel, lines), out_shape=(square...]
    ppermute x8 -> x28, waiting for transfers between devices: 17.1 us -> 101 us  [swapped(): return lax.ppermute(block, 'seq', [(i, i ^ by) for i in range(ring)])]
    ppermute x0 -> x10, waiting for transfers between devices: none -> 29.9 us  [flipped(): lax.ppermute(block, axis, [(i, i ^ by) for i in range(lax.axis_size(axis))])]
    ppermute x8 -> x28, starting transfers between devices: 9.27 us -> 32.6 us  [swapped(): return lax.ppermute(block, 'seq', [(i, i ^ by) for i in range(ring)])]
    all_gather x4, waiting for transfers between devices: 22.8 us -> 0.02 us  [the longest x1 0.02 us: local(): lax.all_gather(after(down_weight, feed_columns), 'batch', axis=0, tiled=T...]
    ppermute x0 -> x10, starting transfers between devices: none -> 13.7 us  [flipped(): lax.ppermute(block, axis, [(i, i ^ by) for i in range(lax.axis_size(axis))])]
    unnamed x139 -> x142, local copies, waits for them, and re-layouts: 49.3 us -> 36.1 us
    dot_general x8 -> x6, matrix products: 60.1 us -> 47.1 us  [dot_nn(): lax.dot_general(left, right, (((1,), (0,)), ((), ())), preferred_element_...]
  transfers between devices with their start and end apart: 15 -> 46, of which waited for: 5 -> 26; matrix products, arithmetic and copies ran while one was open for 28% -> 37% of each run, Pallas kernels for 25% -> 28%
where the time goes in v7:
time: 671 us; the launch traced here: 662 us
  Pallas kernels  188 us (28%)
  matrix products  149 us (22%)
  waiting for transfers between devices  146 us (22%)
  local copies, waits for them, and re-layouts  79.1 us (12%)
  starting transfers between devices  47.1 us (7%)
  other arithmetic  37 us (6%)
  between operations  15.7 us (2%)
    pallas_call x2, Pallas kernels, fold(): pl.pallas_call(functools.partial(fold_kernel, finish, len(given)), out_sh...  155 us
    ppermute x28, waiting for transfers between devices, swapped(): return lax.ppermute(block, 'seq', [(i, i ^ by) for i in range(ring)])  101 us
    dot_general x6, matrix products, dot_nt(): lax.dot_general(left, right, (((1,), (1,)), ((), ())), preferred_element_...  54 us
    dot_general x6, matrix products, dot_tn(): lax.dot_general(left, right, (((0,), (0,)), ((), ())), preferred_element_...  47.8 us
    dot_general x6, matrix products, dot_nn(): lax.dot_general(left, right, (((1,), (0,)), ((), ())), preferred_element_...  47.1 us
    unnamed x142, local copies, waits for them, and re-layouts  36.1 us
    ppermute x28, starting transfers between devices, swapped(): return lax.ppermute(block, 'seq', [(i, i ^ by) for i in range(ring)])  32.6 us
    ppermute x10, waiting for transfers between devices, flipped(): lax.ppermute(block, axis, [(i, i ^ by) for i in range(lax.axis_size(axis))])  29.9 us
  transfers between devices with their start and end apart: 46, of which 26 were waited for; matrix products, arithmetic and copies ran while one was open for 37% of the time, Pallas kernels for 28%

profile of v7, /device:TPU:0, one launch (start us, length us, event | category | flops | bytes accessed | tf_op | source)
XLA Modules:
  0.0 662.4 jit_solution(1017290073744764280)
XLA Ops:
  13.1 2.2 constant_dynamic-slice_fusion.26
  15.4 4.0 collective-permute-start.11
  20.6 6.0 collective-permute-done.11
  26.5 4.7 collective-permute-done.10
  34.0 3.0 constant_dynamic-slice_fusion.17
  37.0 1.8 collective-permute-start.18
  40.8 8.5 %collective-permute-done.18 = bf16[64,2816]{1,0:T(8,128)(2,1)S(1)} collective-permute-done((bf16[64,2816]{1,0:T(8,128)(2,1)S(1)}, bf16[64,2816]{1,0:T(8,128)(2,1)S(1)}, u32[]{:S(2)}, u32[]{:S(2)}) %collective-permute-start.18) | collective-permute-done | bytes 360480 | tf_op jit(solution)/shard_map/ppermute | solution.py:542
  49.3 6.5 collective-permute-done.17
  61.5 2.2 collective-permute-done.5
  63.7 2.6 collective-permute-start.6
  66.3 4.9 collective-permute-done.6
  79.7 18.7 %collective-permute-done.8 = bf16[16,1608]{1,0:T(8,128)(2,1)S(1)} collective-permute-done((bf16[16,1608]{1,0:T(8,128)(2,1)S(1)}, bf16[16,1608]{1,0:T(8,128)(2,1)S(1)}, u32[]{:S(2)}, u32[]{:S(2)}) %collective-permute-start.8) | collective-permute-done | bytes 51488 | tf_op jit(solution)/shard_map/ppermute | solution.py:574
  99.8 1.9 slice.144
  106.4 2.3 constant_dynamic-update-slice_fusion.3
  108.7 2.5 constant_dynamic-update-slice_fusion.2
  111.2 1.9 constant_dynamic-update-slice_fusion.1
  113.1 1.7 collective-permute-done.3
  115.6 3.2 fusion.4
  124.4 16.5 %collective-permute-done.13 = bf16[256,2048]{1,0:T(8,128)(2,1)S(1)} collective-permute-done((bf16[256,2048]{1,0:T(8,128)(2,1)S(1)}, bf16[256,2048]{1,0:T(8,128)(2,1)S(1)}, u32[]{:S(2)}, u32[]{:S(2)}) %collective-permute-start.13) | collective-permute-done | bytes 1048608 | tf_op jit(solution)/shard_map/ppermute | solution.py:542
  141.0 1.9 collective-permute-start.14
  146.5 3.7 collective-permute-done.14
  151.0 1.9 collective-permute-done.15
  153.8 12.7 %fusion.48 = (bf16[1024,2048]{1,0:T(8,128)(2,1)S(1)}, f32[1024,2048]{1,0:T(8,128)S(1)}) fusion(bf16[2048,2048]{1,0:T(8,128)(2,1)} %all-gather.7.cloned.1.call-done, bf16[1024,2048]{1,0:T(8,128)(2,1)} %constant_dynamic-update-slice_fusion, f32[2048]{0:T(1024)S(1)} %reshape.409, f32[1024]{0:T(1024)S(1)} %add_rsqrt_fusion.1), kind=kOutput, calls=%fused_computation.223 | convolution fusion | flops 8600420352 | bytes 25178112 | tf_op jit(solution)/shard_map/dot_general | solution.py:25
  166.6 11.9 %mixer_forward.1 = (f32[1024,512]{1,0:T(8,128)S(1)}, f32[128,1024]{1,0:T(8,128)S(1)}, f32[8,128,512]{2,1,0:T(8,128)S(1)}) custom-call(s32[1]{0:T(128)} %bitcast.mine, bf16[1024,2048]{1,0:T(8,128)(2,1)S(1)} %get-tuple-element.178.query.key.value, bf16[1024,2048]{1,0:T(8,128)(2,1)S(1)} %get-tuple-element.178.query.key.value, ...), custom_call_target="tpu_custom_call" | custom-call | flops 1048576000 | bytes 6291456 | tf_op jit(solution)/shard_map/mixer_forward/pallas_call | solution.py:285
  181.1 2.3 convolution_convert_fusion.5
  183.5 81.0 %fold_forward.1 = (bf16[4,256,2048]{2,1,0:T(8,128)(2,1)S(1)}, f32[256,2048]{1,0:T(8,128)S(1)}) custom-call(bf16[4,256,2048]{2,1,0:T(8,128)(2,1)S(1)} %bitcast.178, bf16[256,2048]{1,0:T(8,128)(2,1)S(1)} %bitcast.177, f32[1,2048]{1,0:T(1,128)S(1)} %reshape.412.refs_2_.refs_3_), custom_call_target="tpu_custom_call" | custom-call | tf_op jit(solution)/shard_map/fold_forward/pallas_call | solution.py:521
  265.8 2.0 copy-done.19
  267.8 17.3 %fusion.49 = f32[1024,2816]{1,0:T(8,128)S(1)} fusion(bf16[1024,2048]{1,0:T(8,128)(2,1)} %bitcast.186, bf16[2048,2816]{1,0:T(8,128)(2,1)} %all-gather.9.cloned.1.call-done), kind=kOutput, calls=%fused_computation.224 | convolution fusion | flops 11811160064 | bytes 27262976 | tf_op jit(solution)/shard_map/dot_general | solution.py:25
  285.1 1.8 multiply_convert_fusion.2
  286.9 2.3 copy-done.26
  290.9 10.7 %convolution_convert_fusion.2 = bf16[1408,2048]{1,0:T(8,128)(2,1)} fusion(bf16[1024,1408]{1,0:T(8,128)(2,1)S(1)} %multiply_convert_fusion.2, bf16[1024,2048]{1,0:T(8,128)(2,1)} %constant_dynamic-update-slice_fusion.9), kind=kOutput, calls=%fused_computation.9 | convolution fusion | flops 5908463616 | bytes 12845056 | tf_op jit(solution)/shard_map/dot_general | solution.py:33
  301.8 15.4 %multiply_convert_fusion.1 = (bf16[1024,1408]{1,0:T(8,128)(2,1)S(1)}, bf16[1024,1408]{1,0:T(8,128)(2,1)}) fusion(f32[1024,2816]{1,0:T(8,128)} %copy-done.26, bf16[1024,2048]{1,0:T(8,128)(2,1)} %constant_dynamic-update-slice_fusion.9, bf16[1408,2048]{1,0:T(8,128)(2,1)} %all-gather.11.cloned.1.call-done), kind=kOutput, calls=%fused_computation.12 | convolution fusion | flops 5924323328 | bytes 27262976 | tf_op jit(solution)/shard_map/dot_general | solution.py:29
  317.2 17.5 %convolution_convert_fusion.3 = bf16[1024,2048]{1,0:T(8,128)(2,1)} fusion(bf16[2048,2816]{1,0:T(8,128)(2,1)} %all-gather.9.cloned.1.call-done, bf16[1024,1408]{1,0:T(8,128)(2,1)} %get-tuple-element.95, bf16[1024,1408]{1,0:T(8,128)(2,1)S(1)} %get-tuple-element.94), kind=kOutput, calls=%fused_computation.18 | convolution fusion | flops 11824791552 | bytes 21495808 | tf_op jit(solution)/shard_map/dot_general | solution.py:29
  334.7 16.9 %convolution_convert_fusion = bf16[2048,2816]{1,0:T(8,128)(2,1)} fusion(bf16[1024,2048]{1,0:T(8,128)(2,1)S(1)} %bitcast.187, bf16[1024,1408]{1,0:T(8,128)(2,1)} %get-tuple-element.95, bf16[1024,1408]{1,0:T(8,128)(2,1)S(1)} %get-tuple-element.94), kind=kOutput, calls=%fused_computation | convolution fusion | flops 11828461568 | bytes 21495808 | tf_op jit(solution)/shard_map/dot_general | solution.py:33
  351.6 15.1 %reduce-scatter.5.cloned.1.call-done = bf16[176,2048]{1,0:T(8,128)(2,1)} async-done(((bf16[1408,2048]{1,0:T(8,128)(2,1)}), bf16[176,2048]{1,0:T(8,128)(2,1)}) %reduce-scatter.5.cloned.1.call-update) | async-done | bytes 720912 | tf_op jit(solution)/shard_map/reduce_scatter | solution.py:798
  368.3 2.2 copy-done.8
  371.7 74.1 %fold_backward.1 = (bf16[4,256,2048]{2,1,0:T(8,128)(2,1)S(1)}, f32[256,2048]{1,0:T(8,128)S(1)}, f32[1,2048]{1,0:T(1,128)S(1)}) custom-call(bf16[4,256,2048]{2,1,0:T(8,128)(2,1)S(1)} %bitcast.179, bf16[256,2048]{1,0:T(8,128)(2,1)S(1)} %bitcast.183, f32[256,2048]{1,0:T(8,128)S(1)} %copy-done.4, f32[1,2048]{1,0:T(1,128)S(1)} %reshape.412.refs_2_.refs_3_), custom_call_target="tpu_custom_call" | custom-call | tf_op jit(solution)/shard_map/fold_backward/pallas_call | solution.py:521
  445.8 6.4 multiply_reduce_fusion
  452.3 3.0 subtract_convert_fusion
  456.0 21.2 %mixer_backward.1 = (bf16[1024,1536]{1,0:T(8,128)(2,1)S(1)}, f32[64,1024]{1,0:T(8,128)S(1)}) custom-call(s32[1]{0:T(128)} %bitcast.mine, bf16[1024,2048]{1,0:T(8,128)(2,1)S(1)} %copy-done.1, bf16[1024,2048]{1,0:T(8,128)(2,1)S(1)} %copy-done.1, bf16[1024,2048]{1,0:T(8,128)(2,1)S(1)} %copy-done.1, bf16[1024,512]{1,0:T(8,128)(2,1)S(1)} %get-tuple-element.96.grad_output, ...), custom_call_target="tpu_custom_call" | custom-call | flops 2097152000 | bytes 10485760 | tf_op jit(solution)/shard_map/mixer_backward/pallas_call | solution.py:310
  478.9 12.3 %convolution_convert_fusion.1 = bf16[2048,2048]{1,0:T(8,128)(2,1)} fusion(bf16[1024,512]{1,0:T(8,128)(2,1)S(1)} %get-tuple-element.97, bf16[1024,1536]{1,0:T(8,128)(2,1)S(1)} %get-tuple-element.52, bf16[1024,2048]{1,0:T(8,128)(2,1)S(1)} %copy-done.23, f32[2048]{0:T(1024)S(1)} %reshape.409, f32[1024]{0:T(1024)S(1)} %add_rsqrt_fusion.1), kind=kOutput, calls=%fused_computation.8 | convolution fusion | flops 8610906112 | bytes 16789504 | tf_op jit(solution)/shard_map/dot_general | solution.py:33
  493.3 12.4 %fusion.6 = f32[1024,2048]{1,0:T(8,128)S(1)} fusion(bf16[2048,2048]{1,0:T(8,128)(2,1)} %all-gather.7.cloned.1.call-done, bf16[1024,512]{1,0:T(8,128)(2,1)S(1)} %copy-done.32, bf16[1024,1536]{1,0:T(8,128)(2,1)} %copy-done.21), kind=kOutput, calls=%fused_computation.22 | convolution fusion | flops 8598323200 | bytes 20971520 | tf_op jit(solution)/shard_map/dot_general | solution.py:29
  505.8 3.5 fusion.3
  511.2 3.3 fusion.40
  517.6 3.0 collective-permute-done.27
  522.2 11.1 %convolution_convert_fusion.4 = bf16[1024,2048]{1,0:T(8,128)(2,1)} fusion(bf16[1024,1408]{1,0:T(8,128)(2,1)} %copy-done.28, bf16[1408,2048]{1,0:T(8,128)(2,1)} %all-gather.11.cloned.1.call-done), kind=kOutput, calls=%fused_computation.19 | convolution fusion | flops 5907677184 | bytes 12845056 | tf_op jit(solution)/shard_map/dot_general | solution.py:25
  533.3 2.7 collective-permute-start.29
  535.9 3.7 convolution_convert_fusion.6
  541.2 2.7 fusion.46
  549.7 17.5 %collective-permute-done.23 = bf16[128,2048]{1,0:T(8,128)(2,1)S(1)} collective-permute-done((bf16[128,2048]{1,0:T(8,128)(2,1)S(1)}, bf16[128,2048]{1,0:T(8,128)(2,1)S(1)}, u32[]{:S(2)}, u32[]{:S(2)}) %collective-permute-start.23) | collective-permute-done | bytes 524320 | tf_op jit(solution)/shard_map/ppermute | solution.py:542
  573.5 1.9 add_convert_fusion.4
  579.7 15.6 %collective-permute-done.26 = bf16[256,2048]{1,0:T(8,128)(2,1)S(1)} collective-permute-done((bf16[256,2048]{1,0:T(8,128)(2,1)}, bf16[256,2048]{1,0:T(8,128)(2,1)S(1)}, u32[]{:S(2)}, u32[]{:S(2)}) %collective-permute-start.26) | collective-permute-done | bytes 1048608 | tf_op jit(solution)/shard_map/ppermute | solution.py:542
  595.3 2.6 collective-permute-done.24
  597.9 3.4 convert_add_fusion
  601.4 1.9 copy.74
  606.5 3.0 copy.76
  609.5 3.3 fusion.16
  616.5 6.0 collective-permute-done.22
  622.5 3.6 fusion.15
  629.1 2.4 collective-permute-done.35
  640.6 2.7 collective-permute-done.33
  643.7 2.6 reshape.416
  646.4 2.9 copy.117
  653.5 1.8 convert_element_type.346
  (346 shorter events, 104.5 us)
Async XLA Ops:
  7.2 108.5 %all-gather.5.cloned.1.call-start = ((), (), s32[]{:S(2)}) async-start(), calls=%async_computation.4 | async-start | bytes 2359296 | tf_op jit(solution)/shard_map/all_gather | solution.py:695
  7.9 145.9 %all-gather.7.cloned.1.call-start = ((), (), s32[]{:S(2)}) async-start(), calls=%async_computation.5 | async-start | bytes 9437184 | tf_op jit(solution)/shard_map/all_gather | solution.py:699
  15.4 11.1 %collective-permute-start.11 = (bf16[64,2048]{1,0:T(8,128)(2,1)S(1)}, bf16[64,2048]{1,0:T(8,128)(2,1)S(1)}, u32[]{:S(2)}, u32[]{:S(2)}) collective-permute-start(bf16[64,2048]{1,0:T(8,128)(2,1)S(1)} %bitcast.226), channel_id=1, source_target_pairs={{0,24},{8,16},{16,8},{24,0},{1,25},{9,17},{17,9},{25,1},{2,26},{10... | collective-permute-start | bytes 786440 | tf_op jit(solution)/shard_map/ppermute | solution.py:542
  19.5 11.8 %collective-permute-start.10 = (bf16[64,2048]{1,0:T(8,128)(2,1)S(1)}, bf16[64,2048]{1,0:T(8,128)(2,1)S(1)}, u32[]{:S(2)}, u32[]{:S(2)}) collective-permute-start(bf16[64,2048]{1,0:T(8,128)(2,1)S(1)} %bitcast.227), channel_id=1, source_target_pairs={{0,16},{8,24},{16,0},{24,8},{1,17},{9,25},{17,1},{25,9},{2,18},{10... | collective-permute-start | bytes 786440 | tf_op jit(solution)/shard_map/ppermute | solution.py:542
  20.2 12.7 %copy-start.36 = (bf16[64,5632]{1,0:T(8,128)(2,1)S(1)}, bf16[64,5632]{1,0:T(8,128)(2,1)}, u32[]{:S(2)}) copy-start(bf16[64,5632]{1,0:T(8,128)(2,1)} %param.30) | copy-start | bytes 2162692
  20.3 11.3 %collective-permute-start.9 = (bf16[64,2048]{1,0:T(8,128)(2,1)S(1)}, bf16[64,2048]{1,0:T(8,128)(2,1)S(1)}, u32[]{:S(2)}, u32[]{:S(2)}) collective-permute-start(bf16[64,2048]{1,0:T(8,128)(2,1)S(1)} %bitcast.228), channel_id=1, source_target_pairs={{0,8},{8,0},{16,24},{24,16},{1,9},{9,1},{17,25},{25,17},{2,10},{10... | collective-permute-start | bytes 786440 | tf_op jit(solution)/shard_map/ppermute | solution.py:542
  32.9 234.9 %all-gather.9.cloned.1.call-start = ((), (), s32[]{:S(2)}) async-start(), calls=%async_computation.6 | async-start | bytes 12976128 | tf_op jit(solution)/shard_map/all_gather | solution.py:701
  37.0 12.3 %collective-permute-start.18 = (bf16[64,2816]{1,0:T(8,128)(2,1)S(1)}, bf16[64,2816]{1,0:T(8,128)(2,1)S(1)}, u32[]{:S(2)}, u32[]{:S(2)}) collective-permute-start(bf16[64,2816]{1,0:T(8,128)(2,1)S(1)} %bitcast.215), channel_id=1, source_target_pairs={{0,24},{8,16},{16,8},{24,0},{1,25},{9,17},{17,9},{25,1},{2,26},{10... | collective-permute-start | bytes 1081352 | tf_op jit(solution)/shard_map/ppermute | solution.py:542
  38.8 17.0 %collective-permute-start.17 = (bf16[64,2816]{1,0:T(8,128)(2,1)S(1)}, bf16[64,2816]{1,0:T(8,128)(2,1)S(1)}, u32[]{:S(2)}, u32[]{:S(2)}) collective-permute-start(bf16[64,2816]{1,0:T(8,128)(2,1)S(1)} %bitcast.216), channel_id=1, source_target_pairs={{0,16},{8,24},{16,0},{24,8},{1,17},{9,25},{17,1},{25,9},{2,18},{10... | collective-permute-start | bytes 1081352 | tf_op jit(solution)/shard_map/ppermute | solution.py:542
  40.2 16.0 %collective-permute-start.16 = (bf16[64,2816]{1,0:T(8,128)(2,1)S(1)}, bf16[64,2816]{1,0:T(8,128)(2,1)S(1)}, u32[]{:S(2)}, u32[]{:S(2)}) collective-permute-start(bf16[64,2816]{1,0:T(8,128)(2,1)S(1)} %bitcast.217), channel_id=1, source_target_pairs={{0,8},{8,0},{16,24},{24,16},{1,9},{9,1},{17,25},{25,17},{2,10},{10... | collective-permute-start | bytes 1081352 | tf_op jit(solution)/shard_map/ppermute | solution.py:542
  56.4 16.3 %copy-start.2 = (bf16[1,256,2048]{2,1,0:T(8,128)(2,1)S(1)}, bf16[1,256,2048]{2,1,0:T(8,128)(2,1)}, u32[]{:S(2)}) copy-start(bf16[1,256,2048]{2,1,0:T(8,128)(2,1)} %param.17) | copy-start | bytes 3145732
  57.8 244.0 %all-gather.11.cloned.1.call-start = ((), (), s32[]{:S(2)}) async-start(), calls=%async_computation.7 | async-start | bytes 6488064 | tf_op jit(solution)/shard_map/all_gather | solution.py:702
  58.6 1.2 collective-permute-start.4
  59.8 3.8 collective-permute-start.5
  63.7 7.4 %collective-permute-start.6 = (bf16[4,1608]{1,0:T(4,128)(2,1)S(1)}, bf16[4,1608]{1,0:T(4,128)(2,1)S(1)}, u32[]{:S(2)}, u32[]{:S(2)}) collective-permute-start(bf16[4,1608]{1,0:T(4,128)(2,1)S(1)} %pad_maximum_fusion.21), channel_id=1, source_target_pairs={{0,4},{1,5},{2,6},{3,7},{4,0},{5,1},{6,2},{7,3},{8,12},{9,13},{10,... | collective-permute-start | bytes 38600 | tf_op jit(solution)/shard_map/ppermute | solution.py:574
  71.2 6.8 %collective-permute-start.7 = (bf16[8,1608]{1,0:T(8,128)(2,1)S(1)}, bf16[8,1608]{1,0:T(8,128)(2,1)S(1)}, u32[]{:S(2)}, u32[]{:S(2)}) collective-permute-start(bf16[8,1608]{1,0:T(8,128)(2,1)S(1)} %pad_maximum_fusion.20), channel_id=1, source_target_pairs={{0,8},{8,0},{16,24},{24,16},{1,9},{9,1},{17,25},{25,17},{2,10},{10... | collective-permute-start | bytes 77192 | tf_op jit(solution)/shard_map/ppermute | solution.py:574
  73.2 28.5 %copy-start.27 = (bf16[1,256,2048]{1,2,0:T(8,128)(2,1)}, bf16[1,256,2048]{1,2,0:T(8,128)(2,1)S(1)}, u32[]{:S(2)}) copy-start(bf16[1,256,2048]{1,2,0:T(8,128)(2,1)S(1)} %copy.63) | copy-start | bytes 3145732
  75.9 28.6 %collective-permute-start = (bf16[256,2048]{1,0:T(8,128)(2,1)S(1)}, bf16[256,2048]{1,0:T(8,128)(2,1)}, u32[]{:S(2)}, u32[]{:S(2)}) collective-permute-start(bf16[256,2048]{1,0:T(8,128)(2,1)S(1)} %copy.67), channel_id=1, source_target_pairs={{0,8},{8,0},{16,24},{24,16},{1,9},{9,1},{17,25},{25,17},{2,10},{10... | collective-permute-start | bytes 3145736 | tf_op jit(solution)/shard_map/ppermute | solution.py:542
  76.5 23.3 %collective-permute-start.1 = (bf16[256,2048]{1,0:T(8,128)(2,1)S(1)}, bf16[256,2048]{1,0:T(8,128)(2,1)}, u32[]{:S(2)}, u32[]{:S(2)}) collective-permute-start(bf16[256,2048]{1,0:T(8,128)(2,1)S(1)} %copy.67), channel_id=1, source_target_pairs={{0,16},{8,24},{16,0},{24,8},{1,17},{9,25},{17,1},{25,9},{2,18},{10... | collective-permute-start | bytes 3145736 | tf_op jit(solution)/shard_map/ppermute | solution.py:542
  78.0 20.3 %collective-permute-start.8 = (bf16[16,1608]{1,0:T(8,128)(2,1)S(1)}, bf16[16,1608]{1,0:T(8,128)(2,1)S(1)}, u32[]{:S(2)}, u32[]{:S(2)}) collective-permute-start(bf16[16,1608]{1,0:T(8,128)(2,1)S(1)} %pad_maximum_fusion.19), channel_id=1, source_target_pairs={{0,16},{8,24},{16,0},{24,8},{1,17},{9,25},{17,1},{25,9},{2,18},{10... | collective-permute-start | bytes 154376 | tf_op jit(solution)/shard_map/ppermute | solution.py:574
  98.6 12.6 %copy-start.41 = (f32[32,64]{1,0:T(8,128)}, f32[32,64]{1,0:T(8,128)S(1)}, u32[]{:S(2)}) copy-start(f32[32,64]{1,0:T(8,128)S(1)} %get-tuple-element.153) | copy-start | bytes 24580
  101.7 9.5 %collective-permute-start.2 = (bf16[128,2048]{1,0:T(8,128)(2,1)}, bf16[128,2048]{1,0:T(8,128)(2,1)}, u32[]{:S(2)}, u32[]{:S(2)}) collective-permute-start(bf16[128,2048]{1,0:T(8,128)(2,1)} %slice.144), channel_id=1, source_target_pairs={{0,8},{8,0},{16,24},{24,16},{1,9},{9,1},{17,25},{25,17},{2,10},{10... | collective-permute-start | bytes 1572872 | tf_op jit(solution)/shard_map/ppermute | solution.py:542
  104.1 16.9 %copy-start.39 = (bf16[16,2048]{1,0:T(8,128)(2,1)}, bf16[16,2048]{1,0:T(8,128)(2,1)S(1)}, u32[]{:S(2)}) copy-start(bf16[16,2048]{1,0:T(8,128)(2,1)S(1)} %reshape.381) | copy-start | bytes 196612
  104.2 18.1 %copy-start.44 = (bf16[256,16]{1,0:T(8,128)(2,1)}, bf16[256,16]{1,0:T(8,128)(2,1)S(1)}, u32[]{:S(2)}) copy-start(bf16[256,16]{1,0:T(8,128)(2,1)S(1)} %reshape.378) | copy-start | bytes 24580
  104.4 262.2 %reduce-scatter.5.cloned.1.call-start = ((), (), s32[]{:S(2)}) async-start(), calls=%async_computation.8 | async-start | bytes 6488064 | tf_op jit(solution)/shard_map/reduce_scatter | solution.py:798
  105.5 9.2 %collective-permute-start.3 = (bf16[128,2048]{1,0:T(8,128)(2,1)S(1)}, bf16[128,2048]{1,0:T(8,128)(2,1)S(1)}, u32[]{:S(2)}, u32[]{:S(2)}) collective-permute-start(bf16[128,2048]{1,0:T(8,128)(2,1)S(1)} %slice.145), channel_id=1, source_target_pairs={{0,16},{8,24},{16,0},{24,8},{1,17},{9,25},{17,1},{25,9},{2,18},{10... | collective-permute-start | bytes 1572872 | tf_op jit(solution)/shard_map/ppermute | solution.py:542
  118.9 24.8 %collective-permute-start.12 = (bf16[256,2048]{1,0:T(8,128)(2,1)S(1)}, bf16[256,2048]{1,0:T(8,128)(2,1)S(1)}, u32[]{:S(2)}, u32[]{:S(2)}) collective-permute-start(bf16[256,2048]{1,0:T(8,128)(2,1)S(1)} %bitcast.180), channel_id=1, source_target_pairs={{0,8},{8,0},{16,24},{24,16},{1,9},{9,1},{17,25},{25,17},{2,10},{10... | collective-permute-start | bytes 3145736 | tf_op jit(solution)/shard_map/ppermute | solution.py:542
  119.6 21.3 %collective-permute-start.13 = (bf16[256,2048]{1,0:T(8,128)(2,1)S(1)}, bf16[256,2048]{1,0:T(8,128)(2,1)S(1)}, u32[]{:S(2)}, u32[]{:S(2)}) collective-permute-start(bf16[256,2048]{1,0:T(8,128)(2,1)S(1)} %bitcast.181), channel_id=1, source_target_pairs={{0,16},{8,24},{16,0},{24,8},{1,17},{9,25},{17,1},{25,9},{2,18},{10... | collective-permute-start | bytes 3145736 | tf_op jit(solution)/shard_map/ppermute | solution.py:542
  122.3 24.2 %copy-start.45 = (bf16[1024,16]{0,1:T(8,128)(2,1)}, bf16[1024,16]{0,1:T(8,128)(2,1)S(1)}, u32[]{:S(2)}) copy-start(bf16[1024,16]{0,1:T(8,128)(2,1)S(1)} %convolution_convert_fusion.8) | copy-start | bytes 98308
  141.0 9.2 %collective-permute-start.14 = (bf16[128,2048]{1,0:T(8,128)(2,1)S(1)}, bf16[128,2048]{1,0:T(8,128)(2,1)S(1)}, u32[]{:S(2)}, u32[]{:S(2)}) collective-permute-start(bf16[128,2048]{1,0:T(8,128)(2,1)S(1)} %slice.147), channel_id=1, source_target_pairs={{0,8},{8,0},{16,24},{24,16},{1,9},{9,1},{17,25},{25,17},{2,10},{10... | collective-permute-start | bytes 1572872 | tf_op jit(solution)/shard_map/ppermute | solution.py:542
  143.7 9.2 %collective-permute-start.15 = (bf16[128,2048]{1,0:T(8,128)(2,1)S(1)}, bf16[128,2048]{1,0:T(8,128)(2,1)S(1)}, u32[]{:S(2)}, u32[]{:S(2)}) collective-permute-start(bf16[128,2048]{1,0:T(8,128)(2,1)S(1)} %slice.148), channel_id=1, source_target_pairs={{0,16},{8,24},{16,0},{24,8},{1,17},{9,25},{17,1},{25,9},{2,18},{10... | collective-permute-start | bytes 1572872 | tf_op jit(solution)/shard_map/ppermute | solution.py:542
  153.8 12.8 %copy-start.6 = (f32[128,1024]{1,0:T(8,128)S(1)}, f32[128,1024]{1,0:T(8,128)}, u32[]{:S(2)}) copy-start(f32[128,1024]{1,0:T(8,128)} %pad_maximum_fusion.17.rate) | copy-start | bytes 1572868
  301.6 189.7 %reduce-scatter.7.cloned.1.call-start = ((), (), s32[]{:S(2)}) async-start(), calls=%async_computation.9 | async-start | bytes 12976128 | tf_op jit(solution)/shard_map/reduce_scatter | solution.py:800
  317.2 17.5 %copy-start.20 = (bf16[4,256,2048]{2,1,0:T(8,128)(2,1)S(1)}, bf16[4,256,2048]{2,1,0:T(8,128)(2,1)}, u32[]{:S(2)}) copy-start(bf16[4,256,2048]{2,1,0:T(8,128)(2,1)} %copy-done.19) | copy-start | bytes 12582916
  366.7 242.8 %reduce-scatter.9.cloned.1.call-start = ((), (), s32[]{:S(2)}) async-start(), calls=%async_computation.10 | async-start | bytes 9437184 | tf_op jit(solution)/shard_map/reduce_scatter | solution.py:851
  371.7 74.1 %copy-start.54 = (bf16[512,2048]{1,0:T(8,128)(2,1)S(1)}, bf16[512,2048]{1,0:T(8,128)(2,1)}, u32[]{:S(2)}) copy-start(bf16[512,2048]{1,0:T(8,128)(2,1)} %all-gather.5.cloned.1.call-done) | copy-start | bytes 6291460
  455.3 22.0 %copy-start.31 = (bf16[1024,512]{1,0:T(8,128)(2,1)}, bf16[1024,512]{1,0:T(8,128)(2,1)S(1)}, u32[]{:S(2)}) copy-start(bf16[1024,512]{1,0:T(8,128)(2,1)S(1)} %get-tuple-element.97) | copy-start | bytes 3145732
  456.0 22.9 %copy-start.23 = (bf16[1024,2048]{1,0:T(8,128)(2,1)S(1)}, bf16[1024,2048]{1,0:T(8,128)(2,1)}, u32[]{:S(2)}) copy-start(bf16[1024,2048]{1,0:T(8,128)(2,1)} %constant_dynamic-update-slice_fusion) | copy-start | bytes 12582916
  491.3 162.2 %reduce-scatter.11.cloned.1.call-start = ((), (), s32[]{:S(2)}) async-start(), calls=%async_computation.11 | async-start | bytes 2359296 | tf_op jit(solution)/shard_map/reduce_scatter | solution.py:852
  493.3 12.4 %copy-start.24 = (bf16[1024,2048]{1,0:T(8,128)(2,1)S(1)}, bf16[1024,2048]{1,0:T(8,128)(2,1)}, u32[]{:S(2)}) copy-start(bf16[1024,2048]{1,0:T(8,128)(2,1)} %constant_dynamic-update-slice_fusion) | copy-start | bytes 12582916
  493.3 12.4 %copy-start.40 = (bf16[16,2048]{1,0:T(8,128)(2,1)S(1)}, bf16[16,2048]{1,0:T(8,128)(2,1)}, u32[]{:S(2)}) copy-start(bf16[16,2048]{1,0:T(8,128)(2,1)} %copy-done.39) | copy-start | bytes 196612
  516.0 4.6 collective-permute-start.27
  520.6 15.3 %copy-start.18 = (bf16[4,256,2048]{2,1,0:T(8,128)(2,1)S(1)}, bf16[4,256,2048]{2,1,0:T(8,128)(2,1)}, u32[]{:S(2)}) copy-start(bf16[4,256,2048]{2,1,0:T(8,128)(2,1)} %copy-done.17) | copy-start | bytes 12582916
  520.6 15.3 %copy-start.35 = (bf16[1024,512]{1,0:T(8,128)(2,1)S(1)}, bf16[1024,512]{1,0:T(8,128)(2,1)}, u32[]{:S(2)}) copy-start(bf16[1024,512]{1,0:T(8,128)(2,1)} %copy-done.34) | copy-start | bytes 3145732
  520.6 12.6 %collective-permute-start.28 = (f32[8,1352]{1,0:T(8,128)S(1)}, f32[8,1352]{1,0:T(8,128)S(1)}, u32[]{:S(2)}, u32[]{:S(2)}) collective-permute-start(f32[8,1352]{1,0:T(8,128)S(1)} %slice_select_fusion.1), channel_id=1, source_target_pairs={{0,8},{8,0},{16,24},{24,16},{1,9},{9,1},{17,25},{25,17},{2,10},{10... | collective-permute-start | bytes 129800 | tf_op jit(solution)/shard_map/ppermute | solution.py:574
  533.3 6.4 collective-permute-start.29
  539.7 6.2 collective-permute-start.30
  544.0 29.6 %collective-permute-start.19 = (bf16[128,2048]{1,0:T(8,128)(2,1)}, bf16[128,2048]{1,0:T(8,128)(2,1)}, u32[]{:S(2)}, u32[]{:S(2)}) collective-permute-start(bf16[128,2048]{1,0:T(8,128)(2,1)} %get-tuple-element.109), channel_id=1, source_target_pairs={{0,16},{8,24},{16,0},{24,8},{1,17},{9,25},{17,1},{25,9},{2,18},{10... | collective-permute-start | bytes 1572872 | tf_op jit(solution)/shard_map/ppermute | solution.py:542
  544.6 28.9 %collective-permute-start.21 = (bf16[128,2048]{1,0:T(8,128)(2,1)}, bf16[128,2048]{1,0:T(8,128)(2,1)}, u32[]{:S(2)}, u32[]{:S(2)}) collective-permute-start(bf16[128,2048]{1,0:T(8,128)(2,1)} %get-tuple-element.108), channel_id=1, source_target_pairs={{0,8},{8,0},{16,24},{24,16},{1,9},{9,1},{17,25},{25,17},{2,10},{10... | collective-permute-start | bytes 1572872 | tf_op jit(solution)/shard_map/ppermute | solution.py:542
  545.9 2.5 collective-permute-start.31
  546.3 21.0 %collective-permute-start.23 = (bf16[128,2048]{1,0:T(8,128)(2,1)S(1)}, bf16[128,2048]{1,0:T(8,128)(2,1)S(1)}, u32[]{:S(2)}, u32[]{:S(2)}) collective-permute-start(bf16[128,2048]{1,0:T(8,128)(2,1)S(1)} %get-tuple-element.103), channel_id=1, source_target_pairs={{0,16},{8,24},{16,0},{24,8},{1,17},{9,25},{17,1},{25,9},{2,18},{10... | collective-permute-start | bytes 1572872 | tf_op jit(solution)/shard_map/ppermute | solution.py:542
  547.3 20.2 %collective-permute-start.25 = (bf16[128,2048]{1,0:T(8,128)(2,1)S(1)}, bf16[128,2048]{1,0:T(8,128)(2,1)S(1)}, u32[]{:S(2)}, u32[]{:S(2)}) collective-permute-start(bf16[128,2048]{1,0:T(8,128)(2,1)S(1)} %get-tuple-element.102), channel_id=1, source_target_pairs={{0,8},{8,0},{16,24},{24,16},{1,9},{9,1},{17,25},{25,17},{2,10},{10... | collective-permute-start | bytes 1572872 | tf_op jit(solution)/shard_map/ppermute | solution.py:542
  569.0 26.3 %collective-permute-start.26 = (bf16[256,2048]{1,0:T(8,128)(2,1)}, bf16[256,2048]{1,0:T(8,128)(2,1)S(1)}, u32[]{:S(2)}, u32[]{:S(2)}) collective-permute-start(bf16[256,2048]{1,0:T(8,128)(2,1)} %pad_maximum_fusion.15), channel_id=1, source_target_pairs={{0,16},{8,24},{16,0},{24,8},{1,17},{9,25},{17,1},{25,9},{2,18},{10... | collective-permute-start | bytes 3145736 | tf_op jit(solution)/shard_map/ppermute | solution.py:542
  571.5 26.4 %collective-permute-start.24 = (bf16[256,2048]{1,0:T(8,128)(2,1)}, bf16[256,2048]{1,0:T(8,128)(2,1)}, u32[]{:S(2)}, u32[]{:S(2)}) collective-permute-start(bf16[256,2048]{1,0:T(8,128)(2,1)} %pad_maximum_fusion.14), channel_id=1, source_target_pairs={{0,8},{8,0},{16,24},{24,16},{1,9},{9,1},{17,25},{25,17},{2,10},{10... | collective-permute-start | bytes 3145736 | tf_op jit(solution)/shard_map/ppermute | solution.py:542
  576.5 46.0 %collective-permute-start.22 = (bf16[256,2048]{1,0:T(8,128)(2,1)}, bf16[256,2048]{1,0:T(8,128)(2,1)}, u32[]{:S(2)}, u32[]{:S(2)}) collective-permute-start(bf16[256,2048]{1,0:T(8,128)(2,1)} %pad_maximum_fusion.13), channel_id=1, source_target_pairs={{0,16},{8,24},{16,0},{24,8},{1,17},{9,25},{17,1},{25,9},{2,18},{10... | collective-permute-start | bytes 3145736 | tf_op jit(solution)/shard_map/ppermute | solution.py:542
  579.2 43.4 %collective-permute-start.20 = (bf16[256,2048]{1,0:T(8,128)(2,1)}, bf16[256,2048]{1,0:T(8,128)(2,1)}, u32[]{:S(2)}, u32[]{:S(2)}) collective-permute-start(bf16[256,2048]{1,0:T(8,128)(2,1)} %pad_maximum_fusion.12), channel_id=1, source_target_pairs={{0,8},{8,0},{16,24},{24,16},{1,9},{9,1},{17,25},{25,17},{2,10},{10... | collective-permute-start | bytes 3145736 | tf_op jit(solution)/shard_map/ppermute | solution.py:542
  609.5 13.0 %copy-start.5 = (f32[256,2048]{1,0:T(8,128)S(1)}, f32[256,2048]{1,0:T(8,128)}, u32[]{:S(2)}) copy-start(f32[256,2048]{1,0:T(8,128)} %copy-done.3) | copy-start | bytes 6291460
  612.9 13.2 %copy-start.38 = (bf16[176,2048]{1,0:T(8,128)(2,1)S(1)}, bf16[176,2048]{1,0:T(8,128)(2,1)}, u32[]{:S(2)}) copy-start(bf16[176,2048]{1,0:T(8,128)(2,1)} %reduce-scatter.5.cloned.1.call-done) | copy-start | bytes 2162692
  613.0 14.6 %collective-permute-start.37 = (bf16[64,2816]{1,0:T(8,128)(2,1)S(1)}, bf16[64,2816]{1,0:T(8,128)(2,1)S(1)}, u32[]{:S(2)}, u32[]{:S(2)}) collective-permute-start(bf16[64,2816]{1,0:T(8,128)(2,1)S(1)} %get-tuple-element.123), channel_id=1, source_target_pairs={{0,24},{8,16},{16,8},{24,0},{1,25},{9,17},{17,9},{25,1},{2,26},{10... | collective-permute-start | bytes 1081352 | tf_op jit(solution)/shard_map/ppermute | solution.py:542
  614.6 14.5 %collective-permute-start.36 = (bf16[64,2816]{1,0:T(8,128)(2,1)S(1)}, bf16[64,2816]{1,0:T(8,128)(2,1)S(1)}, u32[]{:S(2)}, u32[]{:S(2)}) collective-permute-start(bf16[64,2816]{1,0:T(8,128)(2,1)S(1)} %get-tuple-element.124), channel_id=1, source_target_pairs={{0,16},{8,24},{16,0},{24,8},{1,17},{9,25},{17,1},{25,9},{2,18},{10... | collective-permute-start | bytes 1081352 | tf_op jit(solution)/shard_map/ppermute | solution.py:542
  615.0 16.5 %collective-permute-start.35 = (bf16[64,2816]{1,0:T(8,128)(2,1)S(1)}, bf16[64,2816]{1,0:T(8,128)(2,1)S(1)}, u32[]{:S(2)}, u32[]{:S(2)}) collective-permute-start(bf16[64,2816]{1,0:T(8,128)(2,1)S(1)} %get-tuple-element.125), channel_id=1, source_target_pairs={{0,8},{8,0},{16,24},{24,16},{1,9},{9,1},{17,25},{25,17},{2,10},{10... | collective-permute-start | bytes 1081352 | tf_op jit(solution)/shard_map/ppermute | solution.py:542
  632.8 7.8 %collective-permute-start.34 = (bf16[64,2048]{1,0:T(8,128)(2,1)S(1)}, bf16[64,2048]{1,0:T(8,128)(2,1)S(1)}, u32[]{:S(2)}, u32[]{:S(2)}) collective-permute-start(bf16[64,2048]{1,0:T(8,128)(2,1)S(1)} %get-tuple-element.139), channel_id=1, source_target_pairs={{0,24},{8,16},{16,8},{24,0},{1,25},{9,17},{17,9},{25,1},{2,26},{10... | collective-permute-start | bytes 786440 | tf_op jit(solution)/shard_map/ppermute | solution.py:542
  634.5 8.9 %collective-permute-start.33 = (bf16[64,2048]{1,0:T(8,128)(2,1)S(1)}, bf16[64,2048]{1,0:T(8,128)(2,1)S(1)}, u32[]{:S(2)}, u32[]{:S(2)}) collective-permute-start(bf16[64,2048]{1,0:T(8,128)(2,1)S(1)} %get-tuple-element.140), channel_id=1, source_target_pairs={{0,16},{8,24},{16,0},{24,8},{1,17},{9,25},{17,1},{25,9},{2,18},{10... | collective-permute-start | bytes 786440 | tf_op jit(solution)/shard_map/ppermute | solution.py:542
  635.0 8.3 %collective-permute-start.32 = (bf16[64,2048]{1,0:T(8,128)(2,1)S(1)}, bf16[64,2048]{1,0:T(8,128)(2,1)S(1)}, u32[]{:S(2)}, u32[]{:S(2)}) collective-permute-start(bf16[64,2048]{1,0:T(8,128)(2,1)S(1)} %get-tuple-element.141), channel_id=1, source_target_pairs={{0,8},{8,0},{16,24},{24,16},{1,9},{9,1},{17,25},{25,17},{2,10},{10... | collective-permute-start | bytes 786440 | tf_op jit(solution)/shard_map/ppermute | solution.py:542
  (38 other events, 140.8 us)
Sparse Core Ops, SparseCore 0:
  9.6 31.7 all-gather.4
  43.6 82.0 all-gather.6
  128.0 106.4 all-gather.8
  236.0 58.7 all-gather.10
  301.7 64.8 reduce-scatter.4
  368.8 117.6 reduce-scatter.6
  491.4 90.3 reduce-scatter.8
  609.6 33.5 reduce-scatter.10

commit v8 on v7

--- a/solution.py
+++ b/solution.py
@@ -594,6 +594,39 @@
         block = jnp.where(first, low, high) + flipped(jnp.where(first, high, low), axis, by)
         by //= 2
     return block
+
+
+def core_halves(array, lines, axis):
+    size = array.shape[axis] // lines
+    even, odd = (
+        jnp.concatenate(
+            [
+                lax.slice_in_dim(array, line * size, (line + 1) * size, axis=axis)
+                for line in range(which, lines, 2)
+            ],
+            axis=axis,
+        )
+        for which in range(2)
+    )
+    first = lax.axis_index("batch") % 2 == 0
+    return jnp.where(first, even, odd), jnp.where(first, odd, even)
+
+
+def core_sum(features, grads, lines, fill=()):
+    if (features.shape[1] // lines) % 128:
+        mine, others = core_halves(dot_tn(features, grads).astype(BF16), lines, 0)
+        return added(mine, flipped(others, "batch", 1))
+    mine, others = core_halves(features, lines, 1)
+    sent = flipped(dot_tn(others, grads).astype(BF16), "batch", 1)
+    mine = after(mine, *fill) if fill else mine
+    return (dot_tn(mine, grads) + sent.astype(F32)).astype(BF16)
+
+
+def line_sum(terms, lines):
+    groups = [list(range(core, lines, 2)) for core in range(2)]
+    return lax.psum_scatter(
+        terms, "batch", scatter_dimension=0, axis_index_groups=groups, tiled=True
+    )
 
 
 def after(value, *others):
@@ -703,12 +736,9 @@
     if ring != 4:
         w_feed = w_feed.reshape(lines, ring, own, -1).transpose(1, 0, 2, 3).reshape(width, -1)
 
-    def line_major(term):
-        return term.reshape(ring, lines, own, -1).transpose(1, 0, 2, 3).reshape(width, -1)
-
     inputs = after(gathered(permuted(input_own), ring), w_output)
     small = doubled(doubled(params[None], "batch"), "seq")
-    grad_out = gathered(after(grad_own, inputs), ring)
+    grad_out = gathered(after(grad_own, inputs, w_mixer), ring)
     small = small.reshape(devices, -1)
     segment = lax.dynamic_index_in_dim(
         small.reshape(ring, lines, -1), lax.axis_index("batch"), 1, keepdims=False
@@ -757,7 +787,6 @@
     rates = jnp.concatenate([log_rate, -jnp.expm1(log_rate)], axis=0)
     order = mine.reshape(1).astype(jnp.int32)
     mixed, choice, starts = mixer_forward(order, ring, head_size, joined, rates, mask_rows)
-    mixed, grad_out = lax.optimization_barrier((mixed, grad_out))
     head_factor = rms_scale(mixed)
     head_plain = mixed * head_factor
     head_normed = head_plain * gain_head
@@ -765,6 +794,7 @@
     swish_act = swish_pre * swish_sig
     gated = own_part((head_normed * swish_act).astype(BF16))
     terms = dot_nn(gated, w_output).astype(BF16)
+    terms, grad_out = lax.optimization_barrier((terms, grad_out))
     if ring == 4:
         feed_in, hidden = fold(
             finish_forward,
@@ -791,15 +821,11 @@
         [grad_gatepre.astype(BF16), (grad_inner * gate_act).astype(BF16)], axis=1
     )
     back_feedin = dot_nt(grad_feedpre, w_feed).astype(BF16)
-    term_feedpre = dot_tn(after(feed_in, back_feedin), grad_feedpre).astype(BF16)
-    result_terms = dot_nn(inner, w_down).astype(BF16)
-    result = hidden + scattered(result_terms, ring)
-    layer_output = result.astype(BF16).reshape(1, rows, width)
+    result_terms = dot_nn(after(inner, back_feedin), w_down).astype(BF16)
+    feed_lines = feed_in if ring == 4 else permuted(feed_in)
+    term_feedpre = core_sum(after(feed_lines, back_feedin), grad_feedpre, lines, (result_terms,))
     down_share = lax.psum_scatter(term_down, "batch", scatter_dimension=0, tiled=True)
-    feed_terms = term_feedpre if ring == 4 else line_major(term_feedpre)
-    feed_sum = lax.psum_scatter(
-        after(feed_terms, down_share), "batch", scatter_dimension=0, tiled=True
-    )
+    feed_sum = line_sum(after(term_feedpre, down_share), lines)
     if ring == 4:
         grad_branch, grad_hidden, term_feed = fold(
             finish_backward,
@@ -824,8 +850,11 @@
         )
         grad_branch = gathered(grad_hidden.astype(BF16), ring)
 
+    result = hidden + scattered(after(result_terms, grad_branch), ring)
+    layer_output = result.astype(BF16).reshape(1, rows, width)
+
     grad_gated = whole_head(dot_nt(grad_branch, w_output))
-    term_output = dot_tn(gated, grad_branch).astype(BF16)
+    term_output = core_sum(gated, grad_branch, lines)
 
     slope = swish_sig * (1.0 + swish_pre * (1.0 - swish_sig))
     grad_swishpre = own_part((grad_gated * head_normed * slope).astype(BF16))
@@ -847,12 +876,24 @@
             [own_part(grad_pre[:, at * head_size : (at + 1) * head_size]) for at in range(3)], axis=1
         )
     grad_pre = jnp.concatenate([grad_pre, grad_swishpre], axis=1)
-    term_pre = dot_tn(normed, grad_pre).astype(BF16)
-    pre_sum = lax.psum_scatter(after(term_pre, feed_sum), "batch", scatter_dimension=0, tiled=True)
-    output_share = lax.psum_scatter(
-        after(term_output, pre_sum), "batch", scatter_dimension=0, tiled=True
-    )
-    grad_normed = dot_nt(grad_pre, w_mixer) + dot_nn(grad_reduced, w_squeeze)
+    normed_own, normed_other = core_halves(normed, lines, 1)
+    term_other = dot_tn(normed_other, grad_pre).astype(BF16)
+    term_sent = flipped(term_other, "batch", 1)
+    grad_sent, normed_own = lax.optimization_barrier(
+        (grad_pre, normed_own, term_other, feed_sum)
+    )[:2]
+    grad_normed = dot_nt(grad_sent, w_mixer) + dot_nn(grad_reduced, w_squeeze)
+    term_pre = dot_tn(after(normed_own, grad_normed), grad_pre) + term_sent.astype(F32)
+    term_pre = term_pre.astype(BF16)
+    if 4 * part == width:
+        chips = lines // 2
+        joint = jnp.concatenate(
+            [term_pre.reshape(chips, ring * own, width), term_output.reshape(chips, own, width)], axis=1
+        )
+        joint = line_sum(after(joint.reshape(-1, width), feed_sum), lines)
+        pre_sum, output_share = joint[: ring * own], joint[ring * own :]
+    else:
+        pre_sum, output_share = line_sum(term_pre, lines), line_sum(term_output, lines)
     term_mixer = restored(jnp.sum(grad_normed * plain_one, axis=0))
     term_squeeze = restored(dot_tn(grad_reduced, normed))
     grad_normed = restored(scattered(grad_normed.astype(BF16), ring))

time: 671 us -> 679 us (1.012)
  waiting for transfers between devices: 146 us -> 126 us
  local copies, waits for them, and re-layouts: 79.1 us -> 91.6 us
  other arithmetic: 37 us -> 49 us
  Pallas kernels: 188 us -> 197 us
    ppermute x28, waiting for transfers between devices: 101 us -> 81.3 us  [swapped(): return lax.ppermute(block, 'seq', [(i, i ^ by) for i in range(ring)])]
    reduce_scatter x1, waiting for transfers between devices: 15.1 us -> 0.01 us  [local(): lax.psum_scatter(term_down, 'batch', scatter_dimension=0, tiled=True)]
    reduce_scatter x3 -> x2, waiting for transfers between devices: 0.01 us -> 12.1 us  [line_sum(): lax.psum_scatter(terms, 'batch', scatter_dimension=0, axis_index_groups=g...]
    pallas_call x2, Pallas kernels: 155 us -> 163 us  [fold(): pl.pallas_call(functools.partial(fold_kernel, finish, len(given)), out_sh...]
    unnamed x142 -> x234, local copies, waits for them, and re-layouts: 36.1 us -> 38.3 us
    dot_general x6 -> x8, matrix products: 47.8 us -> 49.9 us  [dot_tn(): lax.dot_general(left, right, (((0,), (0,)), ((), ())), preferred_element_...]
    ppermute x10 -> x13, starting transfers between devices: 13.7 us -> 12.9 us  [flipped(): lax.ppermute(block, axis, [(i, i ^ by) for i in range(lax.axis_size(axis))])]
    ppermute x10 -> x13, waiting for transfers between devices: 29.9 us -> 29.2 us  [flipped(): lax.ppermute(block, axis, [(i, i ^ by) for i in range(lax.axis_size(axis))])]
  transfers between devices with their start and end apart: 46 -> 48, of which waited for: 26 -> 24; matrix products, arithmetic and copies ran while one was open for 37% -> 38% of each run, Pallas kernels for 28% -> 29%
where the time goes in v8:
time: 679 us; the launch traced here: 673 us
  Pallas kernels  197 us (29%)
  matrix products  148 us (22%)
  waiting for transfers between devices  126 us (19%)
  local copies, waits for them, and re-layouts  91.6 us (13%)
  other arithmetic  49 us (7%)
  starting transfers between devices  45.9 us (7%)
  between operations  16.3 us (2%)
    pallas_call x2, Pallas kernels, fold(): pl.pallas_call(functools.partial(fold_kernel, finish, len(given)), out_sh...  163 us
    ppermute x28, waiting for transfers between devices, swapped(): return lax.ppermute(block, 'seq', [(i, i ^ by) for i in range(ring)])  81.3 us
    dot_general x6, matrix products, dot_nt(): lax.dot_general(left, right, (((1,), (1,)), ((), ())), preferred_element_...  51.2 us
    dot_general x8, matrix products, dot_tn(): lax.dot_general(left, right, (((0,), (0,)), ((), ())), preferred_element_...  49.9 us
    dot_general x6, matrix products, dot_nn(): lax.dot_general(left, right, (((1,), (0,)), ((), ())), preferred_element_...  46.6 us
    unnamed x234, local copies, waits for them, and re-layouts  38.3 us
    ppermute x28, starting transfers between devices, swapped(): return lax.ppermute(block, 'seq', [(i, i ^ by) for i in range(ring)])  32.3 us
    ppermute x13, waiting for transfers between devices, flipped(): lax.ppermute(block, axis, [(i, i ^ by) for i in range(lax.axis_size(axis))])  29.2 us
  transfers between devices with their start and end apart: 48, of which 24 were waited for; matrix products, arithmetic and copies ran while one was open for 38% of the time, Pallas kernels for 29%

profile of v8, /device:TPU:0, one launch (start us, length us, event | category | flops | bytes accessed | tf_op | source)
XLA Modules:
  0.0 672.6 jit_solution(16021035110070219507)
XLA Ops:
  13.1 2.2 constant_dynamic-slice_fusion.26
  15.4 4.0 collective-permute-start.11
  20.5 6.0 collective-permute-done.11
  26.5 4.7 collective-permute-done.10
  34.2 3.0 constant_dynamic-slice_fusion.17
  41.0 8.5 %collective-permute-done.18 = bf16[64,2816]{1,0:T(8,128)(2,1)S(1)} collective-permute-done((bf16[64,2816]{1,0:T(8,128)(2,1)S(1)}, bf16[64,2816]{1,0:T(8,128)(2,1)S(1)}, u32[]{:S(2)}, u32[]{:S(2)}) %collective-permute-start.18) | collective-permute-done | bytes 360480 | tf_op jit(solution)/shard_map/ppermute | solution.py:542
  49.5 6.6 collective-permute-done.17
  61.7 2.2 collective-permute-done.5
  64.0 2.5 collective-permute-start.6
  66.5 4.6 collective-permute-done.6
  79.7 19.1 %collective-permute-done.8 = bf16[16,1608]{1,0:T(8,128)(2,1)S(1)} collective-permute-done((bf16[16,1608]{1,0:T(8,128)(2,1)S(1)}, bf16[16,1608]{1,0:T(8,128)(2,1)S(1)}, u32[]{:S(2)}, u32[]{:S(2)}) %collective-permute-start.8) | collective-permute-done | bytes 51488 | tf_op jit(solution)/shard_map/ppermute | solution.py:574
  100.2 1.9 slice.248
  106.4 2.3 constant_dynamic-update-slice_fusion.3
  108.8 2.4 constant_dynamic-update-slice_fusion.2
  111.6 1.9 constant_dynamic-update-slice_fusion.1
  115.9 3.2 fusion.4
  123.5 2.3 all-gather.7.cloned.1.call-done
  128.7 12.5 %fusion.50 = (bf16[1024,2048]{1,0:T(8,128)(2,1)S(1)}, f32[1024,2048]{1,0:T(8,128)S(1)}) fusion(bf16[1024,2048]{1,0:T(8,128)(2,1)} %copy-done.18, bf16[2048,2048]{1,0:T(8,128)(2,1)} %all-gather.7.cloned.1.call-done), kind=kOutput, calls=%fused_computation.243 | convolution fusion | flops 8592031744 | bytes 25165824 | tf_op jit(solution)/shard_map/dot_general | solution.py:25
  141.2 11.9 %mixer_forward.1 = (f32[1024,512]{1,0:T(8,128)S(1)}, f32[128,1024]{1,0:T(8,128)S(1)}, f32[8,128,512]{2,1,0:T(8,128)S(1)}) custom-call(s32[1]{0:T(128)} %bitcast.mine, bf16[1024,2048]{1,0:T(8,128)(2,1)S(1)} %get-tuple-element.212.query.key.value, bf16[1024,2048]{1,0:T(8,128)(2,1)S(1)} %get-tuple-element.212.query.key.value, ...), custom_call_target="tpu_custom_call" | custom-call | flops 1048576000 | bytes 6291456 | tf_op jit(solution)/shard_map/mixer_forward/pallas_call | solution.py:285
  155.7 2.3 convolution_convert_fusion.4
  161.1 10.7 %collective-permute-done.14 = bf16[128,2048]{1,0:T(8,128)(2,1)S(1)} collective-permute-done((bf16[128,2048]{1,0:T(8,128)(2,1)S(1)}, bf16[128,2048]{1,0:T(8,128)(2,1)S(1)}, u32[]{:S(2)}, u32[]{:S(2)}) %collective-permute-start.14) | collective-permute-done | bytes 524320 | tf_op jit(solution)/shard_map/ppermute | solution.py:542
  173.6 2.0 copy-done.75
  175.5 85.6 %fold_forward.1 = (bf16[4,256,2048]{2,1,0:T(8,128)(2,1)S(1)}, f32[256,2048]{1,0:T(8,128)S(1)}) custom-call(bf16[4,256,2048]{2,1,0:T(8,128)(2,1)S(1)} %bitcast.186, bf16[256,2048]{1,0:T(8,128)(2,1)S(1)} %bitcast.185, f32[1,2048]{1,0:T(1,128)S(1)} %reshape.424.refs_2_.refs_3_), custom_call_target="tpu_custom_call" | custom-call | tf_op jit(solution)/shard_map/fold_forward/pallas_call | solution.py:521
  262.5 2.0 copy-done.9
  264.4 17.3 %fusion.51 = f32[1024,2816]{1,0:T(8,128)S(1)} fusion(bf16[1024,2048]{1,0:T(8,128)(2,1)} %bitcast.188, bf16[2048,2816]{1,0:T(8,128)(2,1)} %all-gather.9.cloned.1.call-done), kind=kOutput, calls=%fused_computation.244 | convolution fusion | flops 11811160064 | bytes 27262976 | tf_op jit(solution)/shard_map/dot_general | solution.py:25
  281.8 1.8 multiply_convert_fusion.2
  283.6 3.5 copy-done.24
  288.9 8.1 %convolution_convert_fusion = bf16[1408,2048]{1,0:T(8,128)(2,1)} fusion(bf16[1024,1408]{1,0:T(8,128)(2,1)S(1)} %multiply_convert_fusion.2, bf16[1024,2048]{1,0:T(8,128)(2,1)S(1)} %copy-done.76), kind=kOutput, calls=%fused_computation.9 | convolution fusion | flops 5908463616 | bytes 12845056 | tf_op jit(solution)/shard_map/dot_general | solution.py:33
  297.1 15.4 %multiply_convert_fusion.1 = (bf16[1024,1408]{1,0:T(8,128)(2,1)S(1)}, bf16[1024,1408]{1,0:T(8,128)(2,1)}) fusion(f32[1024,2816]{1,0:T(8,128)} %copy-done.24, bf16[1024,2048]{1,0:T(8,128)(2,1)} %copy-done.75, bf16[1408,2048]{1,0:T(8,128)(2,1)} %all-gather.11.cloned.1.call-done), kind=kOutput, calls=%fused_computation.12 | convolution fusion | flops 5924323328 | bytes 27262976 | tf_op jit(solution)/shard_map/dot_general | solution.py:29
  314.1 17.8 %convolution_convert_fusion.2 = bf16[1024,2048]{1,0:T(8,128)(2,1)} fusion(bf16[2048,2816]{1,0:T(8,128)(2,1)} %all-gather.9.cloned.1.call-done, bf16[1024,1408]{1,0:T(8,128)(2,1)} %get-tuple-element.105, bf16[1024,1408]{1,0:T(8,128)(2,1)S(1)} %get-tuple-element.104), kind=kOutput, calls=%fused_computation.20 | convolution fusion | flops 11824791552 | bytes 21495808 | tf_op jit(solution)/shard_map/dot_general | solution.py:29
  332.1 11.5 %convolution_convert_fusion.1 = bf16[1024,2816]{1,0:T(8,128)(2,1)} fusion(pred[]{:T(512)S(6)} %eq.88, bf16[1024,1408]{1,0:T(8,128)(2,1)} %get-tuple-element.105, bf16[1024,1408]{1,0:T(8,128)(2,1)} %copy-done.97, bf16[1024,256]{1,0:T(8,128)(2,1)S(1)} %get-tuple-element.131, bf16[1024,256]{1,0:T(8,128)(2,1)S(1)} %get-tuple-element.132, ...), kind=kOutput, calls=%fused_computation.16 | convolution fusion | flops 5937823744 | bytes 15728641 | tf_op jit(solution)/shard_map/dot_general | solution.py:33
  345.5 11.0 %convolution_convert_fusion.3 = bf16[1024,2048]{1,0:T(8,128)(2,1)} fusion(bf16[1024,1408]{1,0:T(8,128)(2,1)S(1)} %copy-done.30, bf16[1408,2048]{1,0:T(8,128)(2,1)} %all-gather.11.cloned.1.call-done), kind=kOutput, calls=%fused_computation.21 | convolution fusion | flops 5907677184 | bytes 12845056 | tf_op jit(solution)/shard_map/dot_general | solution.py:25
  356.5 8.5 %add_convert_fusion = bf16[1024,2816]{1,0:T(8,128)(2,1)} fusion(bf16[1024,2816]{1,0:T(8,128)(2,1)S(1)} %collective-permute-done.19, bf16[1024,1024]{1,0:T(8,128)(2,1)S(1)} %broadcast_select_fusion.1, bf16[1024,1408]{1,0:T(8,128)(2,1)S(1)} %copy-done.99, bf16[1024,1408]{1,0:T(8,128)(2,1)S(1)} %copy-done.98), kind=kOutput, calls=%fused_computation | convolution fusion | flops 5925765120 | bytes 19398656 | tf_op jit(solution)/shard_map/dot_general | solution.py:33
  366.1 2.5 fusion.45
  371.8 2.1 copy-done.8
  373.9 77.3 %fold_backward.1 = (bf16[4,256,2048]{2,1,0:T(8,128)(2,1)S(1)}, f32[256,2048]{1,0:T(8,128)S(1)}, f32[1,2048]{1,0:T(1,128)S(1)}) custom-call(bf16[4,256,2048]{2,1,0:T(8,128)(2,1)S(1)} %bitcast.187, bf16[256,2048]{1,0:T(8,128)(2,1)} %bitcast.18.refs_1_, f32[256,2048]{1,0:T(8,128)S(1)} %copy-done.4, f32[1,2048]{1,0:T(1,128)S(1)} %reshape.424.refs_2_.refs_3_), custom_call_target="tpu_custom_call" | custom-call | tf_op jit(solution)/shard_map/fold_backward/pallas_call | solution.py:521
  454.7 2.4 convolution_convert_fusion.6
  459.8 3.2 multiply_reduce_fusion
  463.1 2.4 subtract_convert_fusion
  466.5 21.7 %mixer_backward.1 = (bf16[1024,1536]{1,0:T(8,128)(2,1)S(1)}, f32[64,1024]{1,0:T(8,128)S(1)}) custom-call(s32[1]{0:T(128)} %bitcast.mine, bf16[1024,2048]{1,0:T(8,128)(2,1)S(1)} %copy-done.1, bf16[1024,2048]{1,0:T(8,128)(2,1)S(1)} %copy-done.1, bf16[1024,2048]{1,0:T(8,128)(2,1)S(1)} %copy-done.1, bf16[1024,512]{1,0:T(8,128)(2,1)S(1)} %get-tuple-element.106.grad_output, ...), custom_call_target="tpu_custom_call" | custom-call | flops 2097152000 | bytes 10485760 | tf_op jit(solution)/shard_map/mixer_backward/pallas_call | solution.py:310
  488.5 2.1 convolution_convert_fusion.7
  492.0 7.6 %convolution_convert_fusion.5 = bf16[1024,2048]{1,0:T(8,128)(2,1)} fusion(pred[]{:T(512)S(6)} %eq.88, bf16[1024,256]{1,0:T(8,128)(2,1)S(1)} %copy-done.48, bf16[1024,256]{1,0:T(8,128)(2,1)S(1)} %copy-done.50, bf16[1024,256]{1,0:T(8,128)(2,1)S(1)} %copy-done.52, bf16[1024,256]{1,0:T(8,128)(2,1)S(1)} %copy-done.54, bf16[1024,256]{1,0:T(8,128)(2,1)S(1)} %copy-done.56, ...), kind=kOutput, calls=%fused_computation.23 | convolution fusion | flops 4323278848 | bytes 12582913 | tf_op jit(solution)/shard_map/dot_general | solution.py:33
  499.6 2.6 pad_maximum_fusion.2
  507.7 2.1 add_convert_fusion.7
  515.8 12.7 %fusion.52 = f32[1024,2048]{1,0:T(8,128)S(1)} fusion(bf16[1024,2048]{1,0:T(8,128)(2,1)} %pad_maximum_fusion.2, bf16[2048,2048]{1,0:T(8,128)(2,1)} %all-gather.7.cloned.1.call-done), kind=kOutput, calls=%fused_computation.245 | convolution fusion | flops 8589934592 | bytes 20971520 | tf_op jit(solution)/shard_map/dot_general | solution.py:29
  528.6 3.4 fusion.3
  533.6 8.3 %add_convert_fusion.1 = bf16[1024,2048]{1,0:T(8,128)(2,1)S(1)} fusion(bf16[1024,2048]{1,0:T(8,128)(2,1)} %collective-permute-done.33, bf16[1024,1024]{1,0:T(8,128)(2,1)} %broadcast_select_fusion, bf16[1024,512]{1,0:T(8,128)(2,1)S(1)} %copy-done.28, bf16[1024,1536]{1,0:T(8,128)(2,1)} %copy-done.11), kind=kOutput, calls=%fused_computation.8 | convolution fusion | flops 4309647360 | bytes 14680064 | tf_op jit(solution)/shard_map/dot_general | solution.py:33
  541.9 2.8 pad_maximum_fusion.1
  546.9 2.1 collective-permute-done.29
  549.0 2.5 collective-permute-start.30
  551.5 3.7 fusion.19
  573.2 10.5 %collective-permute-done.40 = bf16[64,2816]{1,0:T(8,128)(2,1)} collective-permute-done((bf16[64,2816]{1,0:T(8,128)(2,1)}, bf16[64,2816]{1,0:T(8,128)(2,1)}, u32[]{:S(2)}, u32[]{:S(2)}) %collective-permute-start.40) | collective-permute-done | bytes 360480 | tf_op jit(solution)/shard_map/ppermute | solution.py:542
  583.7 2.7 collective-permute-done.39
  595.2 15.9 %collective-permute-done.27 = bf16[256,2048]{1,0:T(8,128)(2,1)S(1)} collective-permute-done((bf16[256,2048]{1,0:T(8,128)(2,1)S(1)}, bf16[256,2048]{1,0:T(8,128)(2,1)S(1)}, u32[]{:S(2)}, u32[]{:S(2)}) %collective-permute-start.27) | collective-permute-done | bytes 1048608 | tf_op jit(solution)/shard_map/ppermute | solution.py:542
  612.6 3.2 convert_add_fusion
  615.8 1.9 copy.74
  619.8 3.1 copy.76
  623.0 2.4 fusion.11
  627.1 12.1 %reduce-scatter.8.cloned.1.call-done = bf16[320,2048]{1,0:T(8,128)(2,1)} async-done(((bf16[1280,2048]{1,0:T(8,128)(2,1)}), bf16[320,2048]{1,0:T(8,128)(2,1)}) %reduce-scatter.8.cloned.1.call-update) | async-done | bytes 1310736 | tf_op jit(solution)/shard_map/reduce_scatter | solution.py:627
  640.6 2.2 collective-permute-start.37
  646.0 4.9 collective-permute-done.37
  650.8 4.5 collective-permute-done.36
  655.8 2.6 reshape.428
  658.4 2.9 copy.117
  (455 shorter events, 126.8 us)
Async XLA Ops:
  7.2 108.7 %all-gather.5.cloned.1.call-start = ((), (), s32[]{:S(2)}) async-start(), calls=%async_computation.3 | async-start | bytes 2359296 | tf_op jit(solution)/shard_map/all_gather | solution.py:728
  7.9 117.9 %all-gather.7.cloned.1.call-start = ((), (), s32[]{:S(2)}) async-start(), calls=%async_computation.4 | async-start | bytes 9437184 | tf_op jit(solution)/shard_map/all_gather | solution.py:732
  15.4 11.1 %collective-permute-start.11 = (bf16[64,2048]{1,0:T(8,128)(2,1)S(1)}, bf16[64,2048]{1,0:T(8,128)(2,1)S(1)}, u32[]{:S(2)}, u32[]{:S(2)}) collective-permute-start(bf16[64,2048]{1,0:T(8,128)(2,1)S(1)} %bitcast.232), channel_id=1, source_target_pairs={{0,24},{8,16},{16,8},{24,0},{1,25},{9,17},{17,9},{25,1},{2,26},{10... | collective-permute-start | bytes 786440 | tf_op jit(solution)/shard_map/ppermute | solution.py:542
  19.5 11.8 %collective-permute-start.10 = (bf16[64,2048]{1,0:T(8,128)(2,1)S(1)}, bf16[64,2048]{1,0:T(8,128)(2,1)S(1)}, u32[]{:S(2)}, u32[]{:S(2)}) collective-permute-start(bf16[64,2048]{1,0:T(8,128)(2,1)S(1)} %bitcast.233), channel_id=1, source_target_pairs={{0,16},{8,24},{16,0},{24,8},{1,17},{9,25},{17,1},{25,9},{2,18},{10... | collective-permute-start | bytes 786440 | tf_op jit(solution)/shard_map/ppermute | solution.py:542
  20.2 11.3 %collective-permute-start.9 = (bf16[64,2048]{1,0:T(8,128)(2,1)S(1)}, bf16[64,2048]{1,0:T(8,128)(2,1)S(1)}, u32[]{:S(2)}, u32[]{:S(2)}) collective-permute-start(bf16[64,2048]{1,0:T(8,128)(2,1)S(1)} %bitcast.234), channel_id=1, source_target_pairs={{0,8},{8,0},{16,24},{24,16},{1,9},{9,1},{17,25},{25,17},{2,10},{10... | collective-permute-start | bytes 786440 | tf_op jit(solution)/shard_map/ppermute | solution.py:542
  33.0 231.4 %all-gather.9.cloned.1.call-start = ((), (), s32[]{:S(2)}) async-start(), calls=%async_computation.5 | async-start | bytes 12976128 | tf_op jit(solution)/shard_map/all_gather | solution.py:734
  37.2 12.3 %collective-permute-start.18 = (bf16[64,2816]{1,0:T(8,128)(2,1)S(1)}, bf16[64,2816]{1,0:T(8,128)(2,1)S(1)}, u32[]{:S(2)}, u32[]{:S(2)}) collective-permute-start(bf16[64,2816]{1,0:T(8,128)(2,1)S(1)} %bitcast.224), channel_id=1, source_target_pairs={{0,24},{8,16},{16,8},{24,0},{1,25},{9,17},{17,9},{25,1},{2,26},{10... | collective-permute-start | bytes 1081352 | tf_op jit(solution)/shard_map/ppermute | solution.py:542
  39.1 17.0 %collective-permute-start.17 = (bf16[64,2816]{1,0:T(8,128)(2,1)S(1)}, bf16[64,2816]{1,0:T(8,128)(2,1)S(1)}, u32[]{:S(2)}, u32[]{:S(2)}) collective-permute-start(bf16[64,2816]{1,0:T(8,128)(2,1)S(1)} %bitcast.225), channel_id=1, source_target_pairs={{0,16},{8,24},{16,0},{24,8},{1,17},{9,25},{17,1},{25,9},{2,18},{10... | collective-permute-start | bytes 1081352 | tf_op jit(solution)/shard_map/ppermute | solution.py:542
  40.4 16.0 %collective-permute-start.16 = (bf16[64,2816]{1,0:T(8,128)(2,1)S(1)}, bf16[64,2816]{1,0:T(8,128)(2,1)S(1)}, u32[]{:S(2)}, u32[]{:S(2)}) collective-permute-start(bf16[64,2816]{1,0:T(8,128)(2,1)S(1)} %bitcast.226), channel_id=1, source_target_pairs={{0,8},{8,0},{16,24},{24,16},{1,9},{9,1},{17,25},{25,17},{2,10},{10... | collective-permute-start | bytes 1081352 | tf_op jit(solution)/shard_map/ppermute | solution.py:542
  56.6 16.1 %copy-start.2 = (bf16[1,256,2048]{2,1,0:T(8,128)(2,1)S(1)}, bf16[1,256,2048]{2,1,0:T(8,128)(2,1)}, u32[]{:S(2)}) copy-start(bf16[1,256,2048]{2,1,0:T(8,128)(2,1)} %param.17) | copy-start | bytes 3145732
  58.1 239.0 %all-gather.11.cloned.1.call-start = ((), (), s32[]{:S(2)}) async-start(), calls=%async_computation.6 | async-start | bytes 6488064 | tf_op jit(solution)/shard_map/all_gather | solution.py:735
  58.9 1.2 collective-permute-start.4
  60.1 3.8 collective-permute-start.5
  64.0 7.1 %collective-permute-start.6 = (bf16[4,1608]{1,0:T(4,128)(2,1)S(1)}, bf16[4,1608]{1,0:T(4,128)(2,1)S(1)}, u32[]{:S(2)}, u32[]{:S(2)}) collective-permute-start(bf16[4,1608]{1,0:T(4,128)(2,1)S(1)} %pad_maximum_fusion.33), channel_id=1, source_target_pairs={{0,4},{1,5},{2,6},{3,7},{4,0},{5,1},{6,2},{7,3},{8,12},{9,13},{10,... | collective-permute-start | bytes 38600 | tf_op jit(solution)/shard_map/ppermute | solution.py:574
  71.2 6.8 %collective-permute-start.7 = (bf16[8,1608]{1,0:T(8,128)(2,1)S(1)}, bf16[8,1608]{1,0:T(8,128)(2,1)S(1)}, u32[]{:S(2)}, u32[]{:S(2)}) collective-permute-start(bf16[8,1608]{1,0:T(8,128)(2,1)S(1)} %pad_maximum_fusion.32), channel_id=1, source_target_pairs={{0,8},{8,0},{16,24},{24,16},{1,9},{9,1},{17,25},{25,17},{2,10},{10... | collective-permute-start | bytes 77192 | tf_op jit(solution)/shard_map/ppermute | solution.py:574
  75.9 28.9 %collective-permute-start = (bf16[256,2048]{1,0:T(8,128)(2,1)S(1)}, bf16[256,2048]{1,0:T(8,128)(2,1)}, u32[]{:S(2)}, u32[]{:S(2)}) collective-permute-start(bf16[256,2048]{1,0:T(8,128)(2,1)S(1)} %copy.67), channel_id=1, source_target_pairs={{0,8},{8,0},{16,24},{24,16},{1,9},{9,1},{17,25},{25,17},{2,10},{10... | collective-permute-start | bytes 3145736 | tf_op jit(solution)/shard_map/ppermute | solution.py:542
  76.5 23.7 %collective-permute-start.1 = (bf16[256,2048]{1,0:T(8,128)(2,1)S(1)}, bf16[256,2048]{1,0:T(8,128)(2,1)}, u32[]{:S(2)}, u32[]{:S(2)}) collective-permute-start(bf16[256,2048]{1,0:T(8,128)(2,1)S(1)} %copy.67), channel_id=1, source_target_pairs={{0,16},{8,24},{16,0},{24,8},{1,17},{9,25},{17,1},{25,9},{2,18},{10... | collective-permute-start | bytes 3145736 | tf_op jit(solution)/shard_map/ppermute | solution.py:542
  78.0 20.7 %collective-permute-start.8 = (bf16[16,1608]{1,0:T(8,128)(2,1)S(1)}, bf16[16,1608]{1,0:T(8,128)(2,1)S(1)}, u32[]{:S(2)}, u32[]{:S(2)}) collective-permute-start(bf16[16,1608]{1,0:T(8,128)(2,1)S(1)} %pad_maximum_fusion.31), channel_id=1, source_target_pairs={{0,16},{8,24},{16,0},{24,8},{1,17},{9,25},{17,1},{25,9},{2,18},{10... | collective-permute-start | bytes 154376 | tf_op jit(solution)/shard_map/ppermute | solution.py:574
  102.1 9.5 %collective-permute-start.2 = (bf16[128,2048]{1,0:T(8,128)(2,1)}, bf16[128,2048]{1,0:T(8,128)(2,1)}, u32[]{:S(2)}, u32[]{:S(2)}) collective-permute-start(bf16[128,2048]{1,0:T(8,128)(2,1)} %slice.248), channel_id=1, source_target_pairs={{0,8},{8,0},{16,24},{24,16},{1,9},{9,1},{17,25},{25,17},{2,10},{10... | collective-permute-start | bytes 1572872 | tf_op jit(solution)/shard_map/ppermute | solution.py:542
  104.4 16.0 %copy-start.69 = (bf16[16,2048]{1,0:T(8,128)(2,1)}, bf16[16,2048]{1,0:T(8,128)(2,1)S(1)}, u32[]{:S(2)}) copy-start(bf16[16,2048]{1,0:T(8,128)(2,1)S(1)} %reshape.390) | copy-start | bytes 196612
  104.5 17.1 %copy-start.80 = (bf16[256,16]{1,0:T(8,128)(2,1)}, bf16[256,16]{1,0:T(8,128)(2,1)S(1)}, u32[]{:S(2)}) copy-start(bf16[256,16]{1,0:T(8,128)(2,1)S(1)} %reshape.387) | copy-start | bytes 24580
  104.7 260.3 %reduce-scatter.4.cloned.1.call-start = ((), (), s32[]{:S(2)}) async-start(), calls=%async_computation.7 | async-start | bytes 6488064 | tf_op jit(solution)/shard_map/reduce_scatter | solution.py:827
  105.8 9.2 %collective-permute-start.3 = (bf16[128,2048]{1,0:T(8,128)(2,1)S(1)}, bf16[128,2048]{1,0:T(8,128)(2,1)S(1)}, u32[]{:S(2)}, u32[]{:S(2)}) collective-permute-start(bf16[128,2048]{1,0:T(8,128)(2,1)S(1)} %slice.249), channel_id=1, source_target_pairs={{0,16},{8,24},{16,0},{24,8},{1,17},{9,25},{17,1},{25,9},{2,18},{10... | collective-permute-start | bytes 1572872 | tf_op jit(solution)/shard_map/ppermute | solution.py:542
  125.8 15.4 %copy-start.6 = (f32[128,1024]{1,0:T(8,128)S(1)}, f32[128,1024]{1,0:T(8,128)}, u32[]{:S(2)}) copy-start(f32[128,1024]{1,0:T(8,128)} %pad_maximum_fusion.25.rate) | copy-start | bytes 1572868
  125.8 34.4 %collective-permute-start.12 = (bf16[256,2048]{1,0:T(8,128)(2,1)}, bf16[256,2048]{1,0:T(8,128)(2,1)S(1)}, u32[]{:S(2)}, u32[]{:S(2)}) collective-permute-start(bf16[256,2048]{1,0:T(8,128)(2,1)} %bitcast.18.refs_1_), channel_id=1, source_target_pairs={{0,8},{8,0},{16,24},{24,16},{1,9},{9,1},{17,25},{25,17},{2,10},{10... | collective-permute-start | bytes 3145736 | tf_op jit(solution)/shard_map/ppermute | solution.py:542
  127.3 30.8 %collective-permute-start.13 = (bf16[256,2048]{1,0:T(8,128)(2,1)}, bf16[256,2048]{1,0:T(8,128)(2,1)S(1)}, u32[]{:S(2)}, u32[]{:S(2)}) collective-permute-start(bf16[256,2048]{1,0:T(8,128)(2,1)} %bitcast.18.refs_1_), channel_id=1, source_target_pairs={{0,16},{8,24},{16,0},{24,8},{1,17},{9,25},{17,1},{25,9},{2,18},{10... | collective-permute-start | bytes 3145736 | tf_op jit(solution)/shard_map/ppermute | solution.py:542
  141.2 12.0 %copy-start = (bf16[1024,2048]{1,0:T(8,128)(2,1)}, bf16[1024,2048]{1,0:T(8,128)(2,1)S(1)}, u32[]{:S(2)}) copy-start(bf16[1024,2048]{1,0:T(8,128)(2,1)S(1)} %get-tuple-element.212.query.key.value) | copy-start | bytes 12582916
  141.2 12.2 %copy-start.60 = (f32[1024,2048]{1,0:T(8,128)}, f32[1024,2048]{1,0:T(8,128)S(1)}, u32[]{:S(2)}) copy-start(f32[1024,2048]{1,0:T(8,128)S(1)} %get-tuple-element.213) | copy-start | bytes 25165828
  158.1 13.6 %collective-permute-start.14 = (bf16[128,2048]{1,0:T(8,128)(2,1)S(1)}, bf16[128,2048]{1,0:T(8,128)(2,1)S(1)}, u32[]{:S(2)}, u32[]{:S(2)}) collective-permute-start(bf16[128,2048]{1,0:T(8,128)(2,1)S(1)} %slice.252), channel_id=1, source_target_pairs={{0,8},{8,0},{16,24},{24,16},{1,9},{9,1},{17,25},{25,17},{2,10},{10... | collective-permute-start | bytes 1572872 | tf_op jit(solution)/shard_map/ppermute | solution.py:542
  160.2 13.3 %collective-permute-start.15 = (bf16[128,2048]{1,0:T(8,128)(2,1)S(1)}, bf16[128,2048]{1,0:T(8,128)(2,1)S(1)}, u32[]{:S(2)}, u32[]{:S(2)}) collective-permute-start(bf16[128,2048]{1,0:T(8,128)(2,1)S(1)} %slice.253), channel_id=1, source_target_pairs={{0,16},{8,24},{16,0},{24,8},{1,17},{9,25},{17,1},{25,9},{2,18},{10... | collective-permute-start | bytes 1572872 | tf_op jit(solution)/shard_map/ppermute | solution.py:542
  297.0 218.8 %reduce-scatter.6.cloned.1.call-start = ((), (), s32[]{:S(2)}) async-start(), calls=%async_computation.8 | async-start | bytes 7208960 | tf_op jit(solution)/shard_map/reduce_scatter | solution.py:627
  314.1 17.8 %copy-start.10 = (bf16[4,256,2048]{2,1,0:T(8,128)(2,1)S(1)}, bf16[4,256,2048]{2,1,0:T(8,128)(2,1)}, u32[]{:S(2)}) copy-start(bf16[4,256,2048]{2,1,0:T(8,128)(2,1)} %copy-done.9) | copy-start | bytes 12582916
  343.6 12.9 %collective-permute-start.19 = (bf16[1024,2816]{1,0:T(8,128)(2,1)}, bf16[1024,2816]{1,0:T(8,128)(2,1)S(1)}, u32[]{:S(2)}, u32[]{:S(2)}) collective-permute-start(bf16[1024,2816]{1,0:T(8,128)(2,1)} %convolution_convert_fusion.1), channel_id=1, source_target_pairs={{0,1},{1,0},{2,3},{3,2},{4,5},{5,4},{6,7},{7,6},{8,9},{9,8},{10,11... | collective-permute-start | bytes 17301512 | tf_op jit(solution)/shard_map/ppermute | solution.py:574
  345.5 11.0 %copy-start.98 = (bf16[1024,1408]{1,0:T(8,128)(2,1)S(1)}, bf16[1024,1408]{1,0:T(8,128)(2,1)}, u32[]{:S(2)}) copy-start(bf16[1024,1408]{1,0:T(8,128)(2,1)} %copy-done.97) | copy-start | bytes 8650756
  345.5 11.0 %copy-start.99 = (bf16[1024,1408]{1,0:T(8,128)(2,1)S(1)}, bf16[1024,1408]{1,0:T(8,128)(2,1)}, u32[]{:S(2)}) copy-start(bf16[1024,1408]{1,0:T(8,128)(2,1)} %get-tuple-element.105) | copy-start | bytes 8650756
  365.0 274.2 %reduce-scatter.8.cloned.1.call-start = ((), (), s32[]{:S(2)}) async-start(), calls=%async_computation.9 | async-start | bytes 6553600 | tf_op jit(solution)/shard_map/reduce_scatter | solution.py:627
  373.9 77.3 %copy-start.27 = (bf16[1024,2048]{1,0:T(8,128)(2,1)S(1)}, bf16[1024,2048]{1,0:T(8,128)(2,1)}, u32[]{:S(2)}) copy-start(bf16[1024,2048]{1,0:T(8,128)(2,1)} %convolution_convert_fusion.3) | copy-start | bytes 12582916
  452.6 55.0 %collective-permute-start.20 = (bf16[128,2048]{1,0:T(8,128)(2,1)}, bf16[128,2048]{1,0:T(8,128)(2,1)}, u32[]{:S(2)}, u32[]{:S(2)}) collective-permute-start(bf16[128,2048]{1,0:T(8,128)(2,1)} %get-tuple-element.127), channel_id=1, source_target_pairs={{0,16},{8,24},{16,0},{24,8},{1,17},{9,25},{17,1},{25,9},{2,18},{10... | collective-permute-start | bytes 1572872 | tf_op jit(solution)/shard_map/ppermute | solution.py:542
  454.1 53.6 %collective-permute-start.22 = (bf16[128,2048]{1,0:T(8,128)(2,1)}, bf16[128,2048]{1,0:T(8,128)(2,1)}, u32[]{:S(2)}, u32[]{:S(2)}) collective-permute-start(bf16[128,2048]{1,0:T(8,128)(2,1)} %get-tuple-element.126), channel_id=1, source_target_pairs={{0,8},{8,0},{16,24},{24,16},{1,9},{9,1},{17,25},{25,17},{2,10},{10... | collective-permute-start | bytes 1572872 | tf_op jit(solution)/shard_map/ppermute | solution.py:542
  458.7 55.2 %collective-permute-start.34 = (bf16[256,2048]{1,0:T(8,128)(2,1)}, bf16[256,2048]{1,0:T(8,128)(2,1)}, u32[]{:S(2)}, u32[]{:S(2)}) collective-permute-start(bf16[256,2048]{1,0:T(8,128)(2,1)} %broadcast_select_fusion.2), channel_id=1, source_target_pairs={{0,1},{1,0},{2,3},{3,2},{4,5},{5,4},{6,7},{7,6},{8,9},{9,8},{10,11... | collective-permute-start | bytes 3145736 | tf_op jit(solution)/shard_map/ppermute | solution.py:574
  466.5 21.8 %copy-start.77 = (f32[64,1024]{1,0:T(8,128)S(1)}, f32[64,1024]{1,0:T(8,128)}, u32[]{:S(2)}) copy-start(f32[64,1024]{1,0:T(8,128)} %get-tuple-element.214) | copy-start | bytes 786436
  466.5 24.1 %copy-start.19 = (bf16[1024,2048]{1,0:T(8,128)(2,1)S(1)}, bf16[1024,2048]{1,0:T(8,128)(2,1)}, u32[]{:S(2)}) copy-start(bf16[1024,2048]{1,0:T(8,128)(2,1)} %copy-done.18) | copy-start | bytes 12582916
  488.2 11.4 %copy-start.11 = (bf16[1024,1536]{1,0:T(8,128)(2,1)}, bf16[1024,1536]{1,0:T(8,128)(2,1)S(1)}, u32[]{:S(2)}) copy-start(bf16[1024,1536]{1,0:T(8,128)(2,1)S(1)} %get-tuple-element.60) | copy-start | bytes 9437188
  507.6 26.0 %collective-permute-start.33 = (bf16[1024,2048]{1,0:T(8,128)(2,1)}, bf16[1024,2048]{1,0:T(8,128)(2,1)}, u32[]{:S(2)}, u32[]{:S(2)}) collective-permute-start(bf16[1024,2048]{1,0:T(8,128)(2,1)} %convolution_convert_fusion.5), channel_id=1, source_target_pairs={{0,1},{1,0},{2,3},{3,2},{4,5},{5,4},{6,7},{7,6},{8,9},{9,8},{10,11... | collective-permute-start | bytes 12582920 | tf_op jit(solution)/shard_map/ppermute | solution.py:574
  510.8 40.7 %collective-permute-start.23 = (bf16[256,2048]{1,0:T(8,128)(2,1)}, bf16[256,2048]{1,0:T(8,128)(2,1)}, u32[]{:S(2)}, u32[]{:S(2)}) collective-permute-start(bf16[256,2048]{1,0:T(8,128)(2,1)} %pad_maximum_fusion.19), channel_id=1, source_target_pairs={{0,16},{8,24},{16,0},{24,8},{1,17},{9,25},{17,1},{25,9},{2,18},{10... | collective-permute-start | bytes 3145736 | tf_op jit(solution)/shard_map/ppermute | solution.py:542
  513.2 38.3 %collective-permute-start.21 = (bf16[256,2048]{1,0:T(8,128)(2,1)}, bf16[256,2048]{1,0:T(8,128)(2,1)}, u32[]{:S(2)}, u32[]{:S(2)}) collective-permute-start(bf16[256,2048]{1,0:T(8,128)(2,1)} %pad_maximum_fusion.18), channel_id=1, source_target_pairs={{0,8},{8,0},{16,24},{24,16},{1,9},{9,1},{17,25},{25,17},{2,10},{10... | collective-permute-start | bytes 3145736 | tf_op jit(solution)/shard_map/ppermute | solution.py:542
  515.7 12.8 %copy-start.70 = (bf16[16,2048]{1,0:T(8,128)(2,1)S(1)}, bf16[16,2048]{1,0:T(8,128)(2,1)}, u32[]{:S(2)}) copy-start(bf16[16,2048]{1,0:T(8,128)(2,1)} %copy-done.69) | copy-start | bytes 196612
  515.8 12.8 %copy-start.82 = (f32[1024]{0:T(1024)S(1)}, f32[1024]{0:T(1024)}, u32[]{:S(2)}) copy-start(f32[1024]{0:T(1024)} %copy-done.81) | copy-start | bytes 12292
  515.8 12.7 %copy-start.21 = (bf16[1024,2048]{1,0:T(8,128)(2,1)S(1)}, bf16[1024,2048]{1,0:T(8,128)(2,1)}, u32[]{:S(2)}) copy-start(bf16[1024,2048]{1,0:T(8,128)(2,1)} %constant_dynamic-update-slice_fusion) | copy-start | bytes 12582916
  532.2 12.6 %collective-permute-start.28 = (f32[16,1352]{1,0:T(8,128)S(1)}, f32[16,1352]{1,0:T(8,128)S(1)}, u32[]{:S(2)}, u32[]{:S(2)}) collective-permute-start(f32[16,1352]{1,0:T(8,128)S(1)} %slice_select_fusion), channel_id=1, source_target_pairs={{0,16},{8,24},{16,0},{24,8},{1,17},{9,25},{17,1},{25,9},{2,18},{10... | collective-permute-start | bytes 259592 | tf_op jit(solution)/shard_map/ppermute | solution.py:574
  544.9 4.1 collective-permute-start.29
  549.0 7.4 %collective-permute-start.30 = (f32[4,1352]{1,0:T(4,128)S(1)}, f32[4,1352]{1,0:T(4,128)S(1)}, u32[]{:S(2)}, u32[]{:S(2)}) collective-permute-start(f32[4,1352]{1,0:T(4,128)S(1)} %slice_select_fusion.2), channel_id=1, source_target_pairs={{0,4},{1,5},{2,6},{3,7},{4,0},{5,1},{6,2},{7,3},{8,12},{9,13},{10,... | collective-permute-start | bytes 64904 | tf_op jit(solution)/shard_map/ppermute | solution.py:574
  556.5 5.4 collective-permute-start.31
  559.4 28.8 %collective-permute-start.24 = (bf16[128,2048]{1,0:T(8,128)(2,1)}, bf16[128,2048]{1,0:T(8,128)(2,1)S(1)}, u32[]{:S(2)}, u32[]{:S(2)}) collective-permute-start(bf16[128,2048]{1,0:T(8,128)(2,1)} %get-tuple-element.113), channel_id=1, source_target_pairs={{0,16},{8,24},{16,0},{24,8},{1,17},{9,25},{17,1},{25,9},{2,18},{10... | collective-permute-start | bytes 1572872 | tf_op jit(solution)/shard_map/ppermute | solution.py:542
  560.4 27.8 %collective-permute-start.26 = (bf16[128,2048]{1,0:T(8,128)(2,1)}, bf16[128,2048]{1,0:T(8,128)(2,1)S(1)}, u32[]{:S(2)}, u32[]{:S(2)}) collective-permute-start(bf16[128,2048]{1,0:T(8,128)(2,1)} %get-tuple-element.112), channel_id=1, source_target_pairs={{0,8},{8,0},{16,24},{24,16},{1,9},{9,1},{17,25},{25,17},{2,10},{10... | collective-permute-start | bytes 1572872 | tf_op jit(solution)/shard_map/ppermute | solution.py:542
  561.9 3.2 collective-permute-start.32
  563.0 20.8 %collective-permute-start.40 = (bf16[64,2816]{1,0:T(8,128)(2,1)}, bf16[64,2816]{1,0:T(8,128)(2,1)}, u32[]{:S(2)}, u32[]{:S(2)}) collective-permute-start(bf16[64,2816]{1,0:T(8,128)(2,1)} %get-tuple-element.157), channel_id=1, source_target_pairs={{0,24},{8,16},{16,8},{24,0},{1,25},{9,17},{17,9},{25,1},{2,26},{10... | collective-permute-start | bytes 1081352 | tf_op jit(solution)/shard_map/ppermute | solution.py:542
  564.0 22.5 %collective-permute-start.39 = (bf16[64,2816]{1,0:T(8,128)(2,1)}, bf16[64,2816]{1,0:T(8,128)(2,1)}, u32[]{:S(2)}, u32[]{:S(2)}) collective-permute-start(bf16[64,2816]{1,0:T(8,128)(2,1)} %get-tuple-element.158), channel_id=1, source_target_pairs={{0,16},{8,24},{16,0},{24,8},{1,17},{9,25},{17,1},{25,9},{2,18},{10... | collective-permute-start | bytes 1081352 | tf_op jit(solution)/shard_map/ppermute | solution.py:542
  565.1 21.7 %collective-permute-start.38 = (bf16[64,2816]{1,0:T(8,128)(2,1)}, bf16[64,2816]{1,0:T(8,128)(2,1)}, u32[]{:S(2)}, u32[]{:S(2)}) collective-permute-start(bf16[64,2816]{1,0:T(8,128)(2,1)} %get-tuple-element.159), channel_id=1, source_target_pairs={{0,8},{8,0},{16,24},{24,16},{1,9},{9,1},{17,25},{25,17},{2,10},{10... | collective-permute-start | bytes 1081352 | tf_op jit(solution)/shard_map/ppermute | solution.py:542
  589.9 21.1 %collective-permute-start.27 = (bf16[256,2048]{1,0:T(8,128)(2,1)S(1)}, bf16[256,2048]{1,0:T(8,128)(2,1)S(1)}, u32[]{:S(2)}, u32[]{:S(2)}) collective-permute-start(bf16[256,2048]{1,0:T(8,128)(2,1)S(1)} %pad_maximum_fusion.21), channel_id=1, source_target_pairs={{0,16},{8,24},{16,0},{24,8},{1,17},{9,25},{17,1},{25,9},{2,18},{10... | collective-permute-start | bytes 3145736 | tf_op jit(solution)/shard_map/ppermute | solution.py:542
  591.5 21.2 %collective-permute-start.25 = (bf16[256,2048]{1,0:T(8,128)(2,1)S(1)}, bf16[256,2048]{1,0:T(8,128)(2,1)S(1)}, u32[]{:S(2)}, u32[]{:S(2)}) collective-permute-start(bf16[256,2048]{1,0:T(8,128)(2,1)S(1)} %pad_maximum_fusion.20), channel_id=1, source_target_pairs={{0,8},{8,0},{16,24},{24,16},{1,9},{9,1},{17,25},{25,17},{2,10},{10... | collective-permute-start | bytes 3145736 | tf_op jit(solution)/shard_map/ppermute | solution.py:542
  640.6 10.2 %collective-permute-start.37 = (bf16[64,2048]{1,0:T(8,128)(2,1)S(1)}, bf16[64,2048]{1,0:T(8,128)(2,1)S(1)}, u32[]{:S(2)}, u32[]{:S(2)}) collective-permute-start(bf16[64,2048]{1,0:T(8,128)(2,1)S(1)} %get-tuple-element.173), channel_id=1, source_target_pairs={{0,24},{8,16},{16,8},{24,0},{1,25},{9,17},{17,9},{25,1},{2,26},{10... | collective-permute-start | bytes 786440 | tf_op jit(solution)/shard_map/ppermute | solution.py:542
  642.9 12.5 %collective-permute-start.36 = (bf16[64,2048]{1,0:T(8,128)(2,1)S(1)}, bf16[64,2048]{1,0:T(8,128)(2,1)S(1)}, u32[]{:S(2)}, u32[]{:S(2)}) collective-permute-start(bf16[64,2048]{1,0:T(8,128)(2,1)S(1)} %get-tuple-element.174), channel_id=1, source_target_pairs={{0,16},{8,24},{16,0},{24,8},{1,17},{9,25},{17,1},{25,9},{2,18},{10... | collective-permute-start | bytes 786440 | tf_op jit(solution)/shard_map/ppermute | solution.py:542
  643.4 11.9 %collective-permute-start.35 = (bf16[64,2048]{1,0:T(8,128)(2,1)S(1)}, bf16[64,2048]{1,0:T(8,128)(2,1)S(1)}, u32[]{:S(2)}, u32[]{:S(2)}) collective-permute-start(bf16[64,2048]{1,0:T(8,128)(2,1)S(1)} %get-tuple-element.175), channel_id=1, source_target_pairs={{0,8},{8,0},{16,24},{24,16},{1,9},{9,1},{17,25},{25,17},{2,10},{10... | collective-permute-start | bytes 786440 | tf_op jit(solution)/shard_map/ppermute | solution.py:542
  (86 other events, 316.5 us)
Sparse Core Ops, SparseCore 0:
  9.6 31.7 all-gather.4
  43.6 82.1 all-gather.6
  128.0 106.4 all-gather.8
  236.0 58.7 all-gather.10
  297.1 64.8 reduce-scatter.3
  365.1 102.2 reduce-scatter.5
  544.9 94.2 reduce-scatter.7

commit v9 on v8

--- a/solution.py
+++ b/solution.py
@@ -551,7 +551,7 @@
     return jnp.concatenate([block, one, two, low, high], axis=0)
 
 
-def scattered(terms, ring):
+def scattered(terms, ring, middle=(), end=()):
     rows = terms.shape[0] // ring
     parts = [terms[by * rows : (by + 1) * rows] for by in range(ring)]
     total = parts[0].astype(F32)
@@ -561,9 +561,12 @@
         return total
     half = rows // 2
     low, high = swapped(parts[3][:half], 1, ring), swapped(parts[3][half:], 2, ring)
+    low, high = lax.optimization_barrier((low, high) + middle)[:2]
     two = jnp.concatenate([added(parts[2][:half], low), parts[2][half:]], axis=0)
     one = jnp.concatenate([parts[1][:half], added(parts[1][half:], high)], axis=0)
-    return total + swapped(one, 1, ring).astype(F32) + swapped(two, 2, ring).astype(F32)
+    one, two = swapped(one, 1, ring), swapped(two, 2, ring)
+    one, two = lax.optimization_barrier((one, two) + end)[:2]
+    return total + one.astype(F32) + two.astype(F32)
 
 
 def added(left, right):
@@ -850,17 +853,16 @@
         )
         grad_branch = gathered(grad_hidden.astype(BF16), ring)
 
-    result = hidden + scattered(after(result_terms, grad_branch), ring)
-    layer_output = result.astype(BF16).reshape(1, rows, width)
-
     grad_gated = whole_head(dot_nt(grad_branch, w_output))
     term_output = core_sum(gated, grad_branch, lines)
+    output_share = line_sum(after(term_output, feed_sum), lines)
 
     slope = swish_sig * (1.0 + swish_pre * (1.0 - swish_sig))
     grad_swishpre = own_part((grad_gated * head_normed * slope).astype(BF16))
     grad_normed_head = grad_gated * swish_act
     term_head = jnp.sum(grad_normed_head * head_plain, axis=0) / copies
     scaled_head = grad_normed_head * gain_head
+    scaled_head = after(scaled_head, term_output)
     grad_mixed = head_factor * scaled_head - mixed * head_factor**3 * jnp.mean(
         scaled_head * mixed, axis=-1, keepdims=True
     )
@@ -876,24 +878,12 @@
             [own_part(grad_pre[:, at * head_size : (at + 1) * head_size]) for at in range(3)], axis=1
         )
     grad_pre = jnp.concatenate([grad_pre, grad_swishpre], axis=1)
-    normed_own, normed_other = core_halves(normed, lines, 1)
-    term_other = dot_tn(normed_other, grad_pre).astype(BF16)
-    term_sent = flipped(term_other, "batch", 1)
-    grad_sent, normed_own = lax.optimization_barrier(
-        (grad_pre, normed_own, term_other, feed_sum)
-    )[:2]
-    grad_normed = dot_nt(grad_sent, w_mixer) + dot_nn(grad_reduced, w_squeeze)
-    term_pre = dot_tn(after(normed_own, grad_normed), grad_pre) + term_sent.astype(F32)
-    term_pre = term_pre.astype(BF16)
-    if 4 * part == width:
-        chips = lines // 2
-        joint = jnp.concatenate(
-            [term_pre.reshape(chips, ring * own, width), term_output.reshape(chips, own, width)], axis=1
-        )
-        joint = line_sum(after(joint.reshape(-1, width), feed_sum), lines)
-        pre_sum, output_share = joint[: ring * own], joint[ring * own :]
-    else:
-        pre_sum, output_share = line_sum(term_pre, lines), line_sum(term_output, lines)
+    term_pre = dot_tn(after(normed, output_share), grad_pre).astype(BF16)
+    pre_sum = lax.psum_scatter(term_pre, "batch", scatter_dimension=0, tiled=True)
+    grad_normed = dot_nt(after(grad_pre, term_pre), w_mixer) + dot_nn(grad_reduced, w_squeeze)
+    result = hidden + scattered(after(result_terms, grad_branch), ring, (term_pre,))
+    layer_output = result.astype(BF16).reshape(1, rows, width)
+    grad_normed = dot_nt(after(grad_pre, term_pre), w_mixer) + dot_nn(grad_reduced, w_squeeze)
     term_mixer = restored(jnp.sum(grad_normed * plain_one, axis=0))
     term_squeeze = restored(dot_tn(grad_reduced, normed))
     grad_normed = restored(scattered(grad_normed.astype(BF16), ring))
@@ -908,7 +898,7 @@
     pre_share = exchanged(pre_sum.reshape(ring, own, 4 * part), mine, ring)
     pre_share = pre_share.reshape(ring, own, 4, part).transpose(2, 1, 0, 3)
     query_share, key_share, value_share, swish_share = pre_share.reshape(4, own, width).astype(F32)
-    feed_share = exchanged(feed_sum.reshape(ring, own, 2 * hidden_part), mine, ring)
+    feed_share = exchanged(after(feed_sum, term_pre).reshape(ring, own, 2 * hidden_part), mine, ring)
     gate_share = feed_share[:, :, :hidden_part].transpose(1, 0, 2).reshape(own, -1).astype(F32)
     up_share = feed_share[:, :, hidden_part:].transpose(1, 0, 2).reshape(own, -1).astype(F32)
 

time: 679 us -> 692 us (1.019)
  waiting for transfers between devices: 126 us -> 143 us
    ppermute x13 -> x12, waiting for transfers between devices: 29.2 us -> 41.1 us  [flipped(): lax.ppermute(block, axis, [(i, i ^ by) for i in range(lax.axis_size(axis))])]
    dot_general x8 -> x7, matrix products: 49.9 us -> 48.1 us  [dot_tn(): lax.dot_general(left, right, (((0,), (0,)), ((), ())), preferred_element_...]
    unnamed x234 -> x162, local copies, waits for them, and re-layouts: 38.3 us -> 39.9 us
  transfers between devices with their start and end apart: 48 -> 48, of which waited for: 24 -> 28; matrix products, arithmetic and copies ran while one was open for 38% -> 34% of each run, Pallas kernels for 29% -> 29%
where the time goes in v9:
time: 692 us; the launch traced here: 684 us
  Pallas kernels  195 us (28%)
  matrix products  148 us (21%)
  waiting for transfers between devices  143 us (21%)
  local copies, waits for them, and re-layouts  92.8 us (13%)
  starting transfers between devices  46.5 us (7%)
  other arithmetic  42.4 us (6%)
  between operations  16.1 us (2%)
    pallas_call x2, Pallas kernels, fold(): pl.pallas_call(functools.partial(fold_kernel, finish, len(given)), out_sh...  162 us
    ppermute x28, waiting for transfers between devices, swapped(): return lax.ppermute(block, 'seq', [(i, i ^ by) for i in range(ring)])  84.4 us
    dot_general x6, matrix products, dot_nt(): lax.dot_general(left, right, (((1,), (1,)), ((), ())), preferred_element_...  53 us
    dot_general x7, matrix products, dot_tn(): lax.dot_general(left, right, (((0,), (0,)), ((), ())), preferred_element_...  48.1 us
    dot_general x6, matrix products, dot_nn(): lax.dot_general(left, right, (((1,), (0,)), ((), ())), preferred_element_...  46.6 us
    ppermute x12, waiting for transfers between devices, flipped(): lax.ppermute(block, axis, [(i, i ^ by) for i in range(lax.axis_size(axis))])  41.1 us
    unnamed x162, local copies, waits for them, and re-layouts  39.9 us
    ppermute x28, starting transfers between devices, swapped(): return lax.ppermute(block, 'seq', [(i, i ^ by) for i in range(ring)])  32.7 us
  transfers between devices with their start and end apart: 48, of which 28 were waited for; matrix products, arithmetic and copies ran while one was open for 34% of the time, Pallas kernels for 29%

profile of v9, /device:TPU:0, one launch (start us, length us, event | category | flops | bytes accessed | tf_op | source)
XLA Modules:
  0.0 683.7 jit_solution(4284167393312991420)
XLA Ops:
  13.1 2.2 constant_dynamic-slice_fusion.26
  15.4 4.0 collective-permute-start.11
  20.5 6.0 collective-permute-done.11
  26.5 4.7 collective-permute-done.10
  34.2 3.0 constant_dynamic-slice_fusion.17
  41.0 8.5 %collective-permute-done.18 = bf16[64,2816]{1,0:T(8,128)(2,1)S(1)} collective-permute-done((bf16[64,2816]{1,0:T(8,128)(2,1)S(1)}, bf16[64,2816]{1,0:T(8,128)(2,1)S(1)}, u32[]{:S(2)}, u32[]{:S(2)}) %collective-permute-start.18) | collective-permute-done | bytes 360480 | tf_op jit(solution)/shard_map/ppermute | solution.py:542
  49.5 6.5 collective-permute-done.17
  61.8 2.2 collective-permute-done.5
  64.0 2.5 collective-permute-start.6
  66.6 4.6 collective-permute-done.6
  79.7 19.1 %collective-permute-done.8 = bf16[16,1608]{1,0:T(8,128)(2,1)S(1)} collective-permute-done((bf16[16,1608]{1,0:T(8,128)(2,1)S(1)}, bf16[16,1608]{1,0:T(8,128)(2,1)S(1)}, u32[]{:S(2)}, u32[]{:S(2)}) %collective-permute-start.8) | collective-permute-done | bytes 51488 | tf_op jit(solution)/shard_map/ppermute | solution.py:577
  100.2 1.9 slice.208
  106.5 2.3 constant_dynamic-update-slice_fusion.3
  108.8 2.4 constant_dynamic-update-slice_fusion.2
  111.6 1.9 constant_dynamic-update-slice_fusion.1
  115.9 3.2 fusion.4
  123.5 2.2 all-gather.7.cloned.1.call-done
  128.7 12.5 %fusion.44 = (bf16[1024,2048]{1,0:T(8,128)(2,1)S(1)}, f32[1024,2048]{1,0:T(8,128)S(1)}) fusion(bf16[1024,2048]{1,0:T(8,128)(2,1)} %copy-done.19, bf16[2048,2048]{1,0:T(8,128)(2,1)} %all-gather.7.cloned.1.call-done), kind=kOutput, calls=%fused_computation.232 | convolution fusion | flops 8592031744 | bytes 25165824 | tf_op jit(solution)/shard_map/dot_general | solution.py:25
  141.2 11.9 %mixer_forward.1 = (f32[1024,512]{1,0:T(8,128)S(1)}, f32[128,1024]{1,0:T(8,128)S(1)}, f32[8,128,512]{2,1,0:T(8,128)S(1)}) custom-call(s32[1]{0:T(128)} %bitcast.mine, bf16[1024,2048]{1,0:T(8,128)(2,1)S(1)} %get-tuple-element.221.query.key.value, bf16[1024,2048]{1,0:T(8,128)(2,1)S(1)} %get-tuple-element.221.query.key.value, ...), custom_call_target="tpu_custom_call" | custom-call | flops 1048576000 | bytes 6291456 | tf_op jit(solution)/shard_map/mixer_forward/pallas_call | solution.py:285
  155.7 2.3 convolution_convert_fusion.5
  161.1 10.7 %collective-permute-done.14 = bf16[128,2048]{1,0:T(8,128)(2,1)S(1)} collective-permute-done((bf16[128,2048]{1,0:T(8,128)(2,1)S(1)}, bf16[128,2048]{1,0:T(8,128)(2,1)S(1)}, u32[]{:S(2)}, u32[]{:S(2)}) %collective-permute-start.14) | collective-permute-done | bytes 524320 | tf_op jit(solution)/shard_map/ppermute | solution.py:542
  173.6 2.0 copy-done.43
  175.5 85.6 %fold_forward.1 = (bf16[4,256,2048]{2,1,0:T(8,128)(2,1)S(1)}, f32[256,2048]{1,0:T(8,128)S(1)}) custom-call(bf16[4,256,2048]{2,1,0:T(8,128)(2,1)S(1)} %bitcast.183, bf16[256,2048]{1,0:T(8,128)(2,1)S(1)} %bitcast.182, f32[1,2048]{1,0:T(1,128)S(1)} %reshape.412.refs_2_.refs_3_), custom_call_target="tpu_custom_call" | custom-call | tf_op jit(solution)/shard_map/fold_forward/pallas_call | solution.py:521
  262.6 2.1 copy-done.9
  264.6 17.3 %fusion.45 = f32[1024,2816]{1,0:T(8,128)S(1)} fusion(bf16[1024,2048]{1,0:T(8,128)(2,1)} %bitcast.185, bf16[2048,2816]{1,0:T(8,128)(2,1)} %all-gather.9.cloned.1.call-done), kind=kOutput, calls=%fused_computation.233 | convolution fusion | flops 11811160064 | bytes 27262976 | tf_op jit(solution)/shard_map/dot_general | solution.py:25
  283.8 3.5 copy-done.23
  288.9 8.1 %convolution_convert_fusion.1 = bf16[1408,2048]{1,0:T(8,128)(2,1)} fusion(bf16[1024,1408]{1,0:T(8,128)(2,1)S(1)} %multiply_convert_fusion.2, bf16[1024,2048]{1,0:T(8,128)(2,1)S(1)} %copy-done.44), kind=kOutput, calls=%fused_computation.9 | convolution fusion | flops 5908463616 | bytes 12845056 | tf_op jit(solution)/shard_map/dot_general | solution.py:33
  297.1 15.4 %multiply_convert_fusion.1 = (bf16[1024,1408]{1,0:T(8,128)(2,1)S(1)}, bf16[1024,1408]{1,0:T(8,128)(2,1)}) fusion(f32[1024,2816]{1,0:T(8,128)} %copy-done.23, bf16[1024,2048]{1,0:T(8,128)(2,1)} %copy-done.43, bf16[1408,2048]{1,0:T(8,128)(2,1)} %all-gather.11.cloned.1.call-done), kind=kOutput, calls=%fused_computation.12 | convolution fusion | flops 5924323328 | bytes 27262976 | tf_op jit(solution)/shard_map/dot_general | solution.py:29
  314.2 17.8 %convolution_convert_fusion.3 = bf16[1024,2048]{1,0:T(8,128)(2,1)} fusion(bf16[2048,2816]{1,0:T(8,128)(2,1)} %all-gather.9.cloned.1.call-done, bf16[1024,1408]{1,0:T(8,128)(2,1)} %get-tuple-element.123, bf16[1024,1408]{1,0:T(8,128)(2,1)S(1)} %get-tuple-element.122), kind=kOutput, calls=%fused_computation.19 | convolution fusion | flops 11824791552 | bytes 21495808 | tf_op jit(solution)/shard_map/dot_general | solution.py:29
  332.3 11.5 %convolution_convert_fusion.2 = bf16[1024,2816]{1,0:T(8,128)(2,1)} fusion(pred[]{:T(512)S(6)} %eq.86, bf16[1024,1408]{1,0:T(8,128)(2,1)} %get-tuple-element.123, bf16[1024,1408]{1,0:T(8,128)(2,1)} %copy-done.63, bf16[1024,256]{1,0:T(8,128)(2,1)S(1)} %get-tuple-element.140, bf16[1024,256]{1,0:T(8,128)(2,1)S(1)} %get-tuple-element.141, ...), kind=kOutput, calls=%fused_computation.16 | convolution fusion | flops 5937823744 | bytes 15728641 | tf_op jit(solution)/shard_map/dot_general | solution.py:33
  345.7 11.1 %convolution_convert_fusion.4 = bf16[1024,2048]{1,0:T(8,128)(2,1)} fusion(bf16[1024,1408]{1,0:T(8,128)(2,1)S(1)} %copy-done.27, bf16[1408,2048]{1,0:T(8,128)(2,1)} %all-gather.11.cloned.1.call-done), kind=kOutput, calls=%fused_computation.20 | convolution fusion | flops 5907677184 | bytes 12845056 | tf_op jit(solution)/shard_map/dot_general | solution.py:25
  356.8 8.6 %add_convert_fusion = bf16[1024,2816]{1,0:T(8,128)(2,1)} fusion(bf16[1024,2816]{1,0:T(8,128)(2,1)S(1)} %collective-permute-done.19, bf16[1024,1024]{1,0:T(8,128)(2,1)S(1)} %broadcast_select_fusion, bf16[1024,1408]{1,0:T(8,128)(2,1)S(1)} %copy-done.65, bf16[1024,1408]{1,0:T(8,128)(2,1)S(1)} %copy-done.64), kind=kOutput, calls=%fused_computation | convolution fusion | flops 5925765120 | bytes 19398656 | tf_op jit(solution)/shard_map/dot_general | solution.py:33
  367.2 2.2 copy-done.8
  369.4 76.7 %fold_backward.1 = (bf16[4,256,2048]{2,1,0:T(8,128)(2,1)S(1)}, f32[256,2048]{1,0:T(8,128)S(1)}, f32[1,2048]{1,0:T(1,128)S(1)}) custom-call(bf16[4,256,2048]{2,1,0:T(8,128)(2,1)S(1)} %bitcast.184, bf16[256,2048]{1,0:T(8,128)(2,1)} %bitcast.18.refs_1_, f32[256,2048]{1,0:T(8,128)S(1)} %copy-done.4, f32[1,2048]{1,0:T(1,128)S(1)} %reshape.412.refs_2_.refs_3_), custom_call_target="tpu_custom_call" | custom-call | tf_op jit(solution)/shard_map/fold_backward/pallas_call | solution.py:521
  446.2 2.4 convolution_convert_fusion.6
  449.5 2.6 collective-permute-done.22
  453.6 14.2 %reduce-scatter.7.cloned.1.call-done = bf16[256,2816]{1,0:T(8,128)(2,1)} async-done(((bf16[1024,2816]{1,0:T(8,128)(2,1)}), bf16[256,2816]{1,0:T(8,128)(2,1)}) %reduce-scatter.7.cloned.1.call-update) | async-done | bytes 1441808 | tf_op jit(solution)/shard_map/reduce_scatter | solution.py:630
  467.9 6.0 broadcast_multiply_fusion
  474.0 3.9 multiply_reduce_fusion
  480.3 21.2 %mixer_backward.1 = (bf16[1024,1536]{1,0:T(8,128)(2,1)S(1)}, f32[64,1024]{1,0:T(8,128)S(1)}) custom-call(s32[1]{0:T(128)} %bitcast.mine, bf16[1024,2048]{1,0:T(8,128)(2,1)S(1)} %copy-done.1, bf16[1024,2048]{1,0:T(8,128)(2,1)S(1)} %copy-done.1, bf16[1024,2048]{1,0:T(8,128)(2,1)S(1)} %copy-done.1, bf16[1024,512]{1,0:T(8,128)(2,1)S(1)} %subtract_convert_fusion.grad_output, ...), custom_call_target="tpu_custom_call" | custom-call | flops 2097152000 | bytes 10485760 | tf_op jit(solution)/shard_map/mixer_backward/pallas_call | solution.py:310
  503.2 13.7 %convolution_convert_fusion = bf16[2048,2048]{1,0:T(8,128)(2,1)} fusion(bf16[1024,2048]{1,0:T(8,128)(2,1)} %copy-done.19, bf16[1024,512]{1,0:T(8,128)(2,1)S(1)} %copy-done.25, bf16[1024,1536]{1,0:T(8,128)(2,1)} %copy-done.11), kind=kOutput, calls=%fused_computation.8 | convolution fusion | flops 8602517504 | bytes 16777216 | tf_op jit(solution)/shard_map/dot_general | solution.py:33
  518.5 2.9 fusion.40
  527.4 2.9 fusion.47
  531.5 2.6 pad_maximum_fusion.1
  535.4 11.5 %fusion.46 = f32[1024,2048]{1,0:T(8,128)S(1)} fusion(bf16[1024,2048]{1,0:T(8,128)(2,1)S(1)} %pad_maximum_fusion.1, bf16[2048,2048]{1,0:T(8,128)(2,1)} %all-gather.7.cloned.1.call-done), kind=kOutput, calls=%fused_computation.234 | convolution fusion | flops 8589934592 | bytes 20971520 | tf_op jit(solution)/shard_map/dot_general | solution.py:29
  547.0 3.2 fusion.3
  551.1 2.7 fusion.39
  557.4 2.4 constant_dynamic-slice_fusion.4
  561.9 8.0 %collective-permute-done.30 = f32[8,1352]{1,0:T(8,128)S(1)} collective-permute-done((f32[8,1352]{1,0:T(8,128)S(1)}, f32[8,1352]{1,0:T(8,128)S(1)}, u32[]{:S(2)}, u32[]{:S(2)}) %collective-permute-start.30) | collective-permute-done | bytes 43296 | tf_op jit(solution)/shard_map/ppermute | solution.py:577
  569.9 3.1 collective-permute-start.31
  573.0 2.0 add_convert_fusion.5
  577.1 2.8 collective-permute-done.32
  594.9 1.9 add_convert_fusion.3
  601.8 14.1 %collective-permute-done.23 = bf16[256,2048]{1,0:T(8,128)(2,1)S(1)} collective-permute-done((bf16[256,2048]{1,0:T(8,128)(2,1)S(1)}, bf16[256,2048]{1,0:T(8,128)(2,1)S(1)}, u32[]{:S(2)}, u32[]{:S(2)}) %collective-permute-start.23) | collective-permute-done | bytes 1048608 | tf_op jit(solution)/shard_map/ppermute | solution.py:542
  617.0 21.0 %collective-permute-done.27 = bf16[256,2048]{1,0:T(8,128)(2,1)S(1)} collective-permute-done((bf16[256,2048]{1,0:T(8,128)(2,1)S(1)}, bf16[256,2048]{1,0:T(8,128)(2,1)S(1)}, u32[]{:S(2)}, u32[]{:S(2)}) %collective-permute-start.27) | collective-permute-done | bytes 1048608 | tf_op jit(solution)/shard_map/ppermute | solution.py:542
  638.4 3.0 convert_add_fusion
  641.4 1.9 copy.68
  645.4 3.1 copy.70
  648.5 2.4 fusion.11
  655.9 4.8 fusion.17
  660.8 1.8 collective-permute-done.36
  662.6 3.8 collective-permute-done.35
  666.9 2.4 reshape.416
  669.3 2.9 copy.110
  (378 shorter events, 119.8 us)
Async XLA Ops:
  7.2 108.8 %all-gather.5.cloned.1.call-start = ((), (), s32[]{:S(2)}) async-start(), calls=%async_computation.4 | async-start | bytes 2359296 | tf_op jit(solution)/shard_map/all_gather | solution.py:731
  7.9 117.9 %all-gather.7.cloned.1.call-start = ((), (), s32[]{:S(2)}) async-start(), calls=%async_computation.5 | async-start | bytes 9437184 | tf_op jit(solution)/shard_map/all_gather | solution.py:735
  15.4 11.1 %collective-permute-start.11 = (bf16[64,2048]{1,0:T(8,128)(2,1)S(1)}, bf16[64,2048]{1,0:T(8,128)(2,1)S(1)}, u32[]{:S(2)}, u32[]{:S(2)}) collective-permute-start(bf16[64,2048]{1,0:T(8,128)(2,1)S(1)} %bitcast.224), channel_id=1, source_target_pairs={{0,24},{8,16},{16,8},{24,0},{1,25},{9,17},{17,9},{25,1},{2,26},{10... | collective-permute-start | bytes 786440 | tf_op jit(solution)/shard_map/ppermute | solution.py:542
  19.5 11.8 %collective-permute-start.10 = (bf16[64,2048]{1,0:T(8,128)(2,1)S(1)}, bf16[64,2048]{1,0:T(8,128)(2,1)S(1)}, u32[]{:S(2)}, u32[]{:S(2)}) collective-permute-start(bf16[64,2048]{1,0:T(8,128)(2,1)S(1)} %bitcast.225), channel_id=1, source_target_pairs={{0,16},{8,24},{16,0},{24,8},{1,17},{9,25},{17,1},{25,9},{2,18},{10... | collective-permute-start | bytes 786440 | tf_op jit(solution)/shard_map/ppermute | solution.py:542
  20.2 11.3 %collective-permute-start.9 = (bf16[64,2048]{1,0:T(8,128)(2,1)S(1)}, bf16[64,2048]{1,0:T(8,128)(2,1)S(1)}, u32[]{:S(2)}, u32[]{:S(2)}) collective-permute-start(bf16[64,2048]{1,0:T(8,128)(2,1)S(1)} %bitcast.226), channel_id=1, source_target_pairs={{0,8},{8,0},{16,24},{24,16},{1,9},{9,1},{17,25},{25,17},{2,10},{10... | collective-permute-start | bytes 786440 | tf_op jit(solution)/shard_map/ppermute | solution.py:542
  33.0 231.7 %all-gather.9.cloned.1.call-start = ((), (), s32[]{:S(2)}) async-start(), calls=%async_computation.6 | async-start | bytes 12976128 | tf_op jit(solution)/shard_map/all_gather | solution.py:737
  37.2 12.3 %collective-permute-start.18 = (bf16[64,2816]{1,0:T(8,128)(2,1)S(1)}, bf16[64,2816]{1,0:T(8,128)(2,1)S(1)}, u32[]{:S(2)}, u32[]{:S(2)}) collective-permute-start(bf16[64,2816]{1,0:T(8,128)(2,1)S(1)} %bitcast.216), channel_id=1, source_target_pairs={{0,24},{8,16},{16,8},{24,0},{1,25},{9,17},{17,9},{25,1},{2,26},{10... | collective-permute-start | bytes 1081352 | tf_op jit(solution)/shard_map/ppermute | solution.py:542
  39.1 17.0 %collective-permute-start.17 = (bf16[64,2816]{1,0:T(8,128)(2,1)S(1)}, bf16[64,2816]{1,0:T(8,128)(2,1)S(1)}, u32[]{:S(2)}, u32[]{:S(2)}) collective-permute-start(bf16[64,2816]{1,0:T(8,128)(2,1)S(1)} %bitcast.217), channel_id=1, source_target_pairs={{0,16},{8,24},{16,0},{24,8},{1,17},{9,25},{17,1},{25,9},{2,18},{10... | collective-permute-start | bytes 1081352 | tf_op jit(solution)/shard_map/ppermute | solution.py:542
  40.4 16.0 %collective-permute-start.16 = (bf16[64,2816]{1,0:T(8,128)(2,1)S(1)}, bf16[64,2816]{1,0:T(8,128)(2,1)S(1)}, u32[]{:S(2)}, u32[]{:S(2)}) collective-permute-start(bf16[64,2816]{1,0:T(8,128)(2,1)S(1)} %bitcast.218), channel_id=1, source_target_pairs={{0,8},{8,0},{16,24},{24,16},{1,9},{9,1},{17,25},{25,17},{2,10},{10... | collective-permute-start | bytes 1081352 | tf_op jit(solution)/shard_map/ppermute | solution.py:542
  56.8 16.0 %copy-start.2 = (bf16[1,256,2048]{2,1,0:T(8,128)(2,1)S(1)}, bf16[1,256,2048]{2,1,0:T(8,128)(2,1)}, u32[]{:S(2)}) copy-start(bf16[1,256,2048]{2,1,0:T(8,128)(2,1)} %param.17) | copy-start | bytes 3145732
  58.1 239.0 %all-gather.11.cloned.1.call-start = ((), (), s32[]{:S(2)}) async-start(), calls=%async_computation.7 | async-start | bytes 6488064 | tf_op jit(solution)/shard_map/all_gather | solution.py:738
  58.9 1.2 collective-permute-start.4
  60.1 3.8 collective-permute-start.5
  64.0 7.1 %collective-permute-start.6 = (bf16[4,1608]{1,0:T(4,128)(2,1)S(1)}, bf16[4,1608]{1,0:T(4,128)(2,1)S(1)}, u32[]{:S(2)}, u32[]{:S(2)}) collective-permute-start(bf16[4,1608]{1,0:T(4,128)(2,1)S(1)} %pad_maximum_fusion.28), channel_id=1, source_target_pairs={{0,4},{1,5},{2,6},{3,7},{4,0},{5,1},{6,2},{7,3},{8,12},{9,13},{10,... | collective-permute-start | bytes 38600 | tf_op jit(solution)/shard_map/ppermute | solution.py:577
  71.2 6.8 collective-permute-start.7
  75.9 28.9 %collective-permute-start = (bf16[256,2048]{1,0:T(8,128)(2,1)S(1)}, bf16[256,2048]{1,0:T(8,128)(2,1)}, u32[]{:S(2)}, u32[]{:S(2)}) collective-permute-start(bf16[256,2048]{1,0:T(8,128)(2,1)S(1)} %copy.63), channel_id=1, source_target_pairs={{0,8},{8,0},{16,24},{24,16},{1,9},{9,1},{17,25},{25,17},{2,10},{10... | collective-permute-start | bytes 3145736 | tf_op jit(solution)/shard_map/ppermute | solution.py:542
  76.5 23.7 %collective-permute-start.1 = (bf16[256,2048]{1,0:T(8,128)(2,1)S(1)}, bf16[256,2048]{1,0:T(8,128)(2,1)}, u32[]{:S(2)}, u32[]{:S(2)}) collective-permute-start(bf16[256,2048]{1,0:T(8,128)(2,1)S(1)} %copy.63), channel_id=1, source_target_pairs={{0,16},{8,24},{16,0},{24,8},{1,17},{9,25},{17,1},{25,9},{2,18},{10... | collective-permute-start | bytes 3145736 | tf_op jit(solution)/shard_map/ppermute | solution.py:542
  78.0 20.7 %collective-permute-start.8 = (bf16[16,1608]{1,0:T(8,128)(2,1)S(1)}, bf16[16,1608]{1,0:T(8,128)(2,1)S(1)}, u32[]{:S(2)}, u32[]{:S(2)}) collective-permute-start(bf16[16,1608]{1,0:T(8,128)(2,1)S(1)} %pad_maximum_fusion.26), channel_id=1, source_target_pairs={{0,16},{8,24},{16,0},{24,8},{1,17},{9,25},{17,1},{25,9},{2,18},{10... | collective-permute-start | bytes 154376 | tf_op jit(solution)/shard_map/ppermute | solution.py:577
  102.1 9.5 %collective-permute-start.2 = (bf16[128,2048]{1,0:T(8,128)(2,1)}, bf16[128,2048]{1,0:T(8,128)(2,1)}, u32[]{:S(2)}, u32[]{:S(2)}) collective-permute-start(bf16[128,2048]{1,0:T(8,128)(2,1)} %slice.208), channel_id=1, source_target_pairs={{0,8},{8,0},{16,24},{24,16},{1,9},{9,1},{17,25},{25,17},{2,10},{10... | collective-permute-start | bytes 1572872 | tf_op jit(solution)/shard_map/ppermute | solution.py:542
  104.4 16.0 %copy-start.38 = (bf16[16,2048]{1,0:T(8,128)(2,1)}, bf16[16,2048]{1,0:T(8,128)(2,1)S(1)}, u32[]{:S(2)}) copy-start(bf16[16,2048]{1,0:T(8,128)(2,1)S(1)} %reshape.381) | copy-start | bytes 196612
  104.6 17.1 %copy-start.48 = (bf16[256,16]{1,0:T(8,128)(2,1)}, bf16[256,16]{1,0:T(8,128)(2,1)S(1)}, u32[]{:S(2)}) copy-start(bf16[256,16]{1,0:T(8,128)(2,1)S(1)} %reshape.378) | copy-start | bytes 24580
  104.7 260.7 %reduce-scatter.5.cloned.1.call-start = ((), (), s32[]{:S(2)}) async-start(), calls=%async_computation.8 | async-start | bytes 6488064 | tf_op jit(solution)/shard_map/reduce_scatter | solution.py:830
  105.9 9.2 %collective-permute-start.3 = (bf16[128,2048]{1,0:T(8,128)(2,1)S(1)}, bf16[128,2048]{1,0:T(8,128)(2,1)S(1)}, u32[]{:S(2)}, u32[]{:S(2)}) collective-permute-start(bf16[128,2048]{1,0:T(8,128)(2,1)S(1)} %slice.209), channel_id=1, source_target_pairs={{0,16},{8,24},{16,0},{24,8},{1,17},{9,25},{17,1},{25,9},{2,18},{10... | collective-permute-start | bytes 1572872 | tf_op jit(solution)/shard_map/ppermute | solution.py:542
  125.8 15.5 %copy-start.6 = (f32[128,1024]{1,0:T(8,128)S(1)}, f32[128,1024]{1,0:T(8,128)}, u32[]{:S(2)}) copy-start(f32[128,1024]{1,0:T(8,128)} %pad_maximum_fusion.22.rate) | copy-start | bytes 1572868
  125.8 34.4 %collective-permute-start.12 = (bf16[256,2048]{1,0:T(8,128)(2,1)}, bf16[256,2048]{1,0:T(8,128)(2,1)S(1)}, u32[]{:S(2)}, u32[]{:S(2)}) collective-permute-start(bf16[256,2048]{1,0:T(8,128)(2,1)} %bitcast.18.refs_1_), channel_id=1, source_target_pairs={{0,8},{8,0},{16,24},{24,16},{1,9},{9,1},{17,25},{25,17},{2,10},{10... | collective-permute-start | bytes 3145736 | tf_op jit(solution)/shard_map/ppermute | solution.py:542
  127.3 30.8 %collective-permute-start.13 = (bf16[256,2048]{1,0:T(8,128)(2,1)}, bf16[256,2048]{1,0:T(8,128)(2,1)S(1)}, u32[]{:S(2)}, u32[]{:S(2)}) collective-permute-start(bf16[256,2048]{1,0:T(8,128)(2,1)} %bitcast.18.refs_1_), channel_id=1, source_target_pairs={{0,16},{8,24},{16,0},{24,8},{1,17},{9,25},{17,1},{25,9},{2,18},{10... | collective-permute-start | bytes 3145736 | tf_op jit(solution)/shard_map/ppermute | solution.py:542
  141.2 12.0 %copy-start = (bf16[1024,2048]{1,0:T(8,128)(2,1)}, bf16[1024,2048]{1,0:T(8,128)(2,1)S(1)}, u32[]{:S(2)}) copy-start(bf16[1024,2048]{1,0:T(8,128)(2,1)S(1)} %get-tuple-element.221.query.key.value) | copy-start | bytes 12582916
  141.2 12.2 %copy-start.28 = (f32[1024,2048]{1,0:T(8,128)}, f32[1024,2048]{1,0:T(8,128)S(1)}, u32[]{:S(2)}) copy-start(f32[1024,2048]{1,0:T(8,128)S(1)} %get-tuple-element.222) | copy-start | bytes 25165828
  158.1 13.6 %collective-permute-start.14 = (bf16[128,2048]{1,0:T(8,128)(2,1)S(1)}, bf16[128,2048]{1,0:T(8,128)(2,1)S(1)}, u32[]{:S(2)}, u32[]{:S(2)}) collective-permute-start(bf16[128,2048]{1,0:T(8,128)(2,1)S(1)} %slice.212), channel_id=1, source_target_pairs={{0,8},{8,0},{16,24},{24,16},{1,9},{9,1},{17,25},{25,17},{2,10},{10... | collective-permute-start | bytes 1572872 | tf_op jit(solution)/shard_map/ppermute | solution.py:542
  160.2 13.3 %collective-permute-start.15 = (bf16[128,2048]{1,0:T(8,128)(2,1)S(1)}, bf16[128,2048]{1,0:T(8,128)(2,1)S(1)}, u32[]{:S(2)}, u32[]{:S(2)}) collective-permute-start(bf16[128,2048]{1,0:T(8,128)(2,1)S(1)} %slice.213), channel_id=1, source_target_pairs={{0,16},{8,24},{16,0},{24,8},{1,17},{9,25},{17,1},{25,9},{2,18},{10... | collective-permute-start | bytes 1572872 | tf_op jit(solution)/shard_map/ppermute | solution.py:542
  297.1 170.8 %reduce-scatter.7.cloned.1.call-start = ((), (), s32[]{:S(2)}) async-start(), calls=%async_computation.9 | async-start | bytes 7208960 | tf_op jit(solution)/shard_map/reduce_scatter | solution.py:630
  314.2 17.8 %copy-start.10 = (bf16[4,256,2048]{2,1,0:T(8,128)(2,1)S(1)}, bf16[4,256,2048]{2,1,0:T(8,128)(2,1)}, u32[]{:S(2)}) copy-start(bf16[4,256,2048]{2,1,0:T(8,128)(2,1)} %copy-done.9) | copy-start | bytes 12582916
  343.8 13.0 %collective-permute-start.19 = (bf16[1024,2816]{1,0:T(8,128)(2,1)}, bf16[1024,2816]{1,0:T(8,128)(2,1)S(1)}, u32[]{:S(2)}, u32[]{:S(2)}) collective-permute-start(bf16[1024,2816]{1,0:T(8,128)(2,1)} %convolution_convert_fusion.2), channel_id=1, source_target_pairs={{0,1},{1,0},{2,3},{3,2},{4,5},{5,4},{6,7},{7,6},{8,9},{9,8},{10,11... | collective-permute-start | bytes 17301512 | tf_op jit(solution)/shard_map/ppermute | solution.py:577
  365.4 137.8 %reduce-scatter.9.cloned.1.call-start = ((), (), s32[]{:S(2)}) async-start(), calls=%async_computation.10 | async-start | bytes 1310720 | tf_op jit(solution)/shard_map/reduce_scatter | solution.py:630
  369.4 76.7 %copy-start.34 = (bf16[1024,512]{1,0:T(8,128)(2,1)S(1)}, bf16[1024,512]{1,0:T(8,128)(2,1)}, u32[]{:S(2)}) copy-start(bf16[1024,512]{1,0:T(8,128)(2,1)} %copy-done.33) | copy-start | bytes 3145732
  449.4 2.7 collective-permute-start.22
  467.8 183.1 %reduce-scatter.11.cloned.1.call-start = ((), (), s32[]{:S(2)}) async-start(), calls=%async_computation.11 | async-start | bytes 9437184 | tf_op jit(solution)/shard_map/reduce_scatter | solution.py:882
  480.3 22.9 %copy-start.25 = (bf16[1024,512]{1,0:T(8,128)(2,1)S(1)}, bf16[1024,512]{1,0:T(8,128)(2,1)}, u32[]{:S(2)}) copy-start(bf16[1024,512]{1,0:T(8,128)(2,1)} %get-tuple-element.124) | copy-start | bytes 3145732
  521.4 32.4 %collective-permute-start.20 = (bf16[128,2048]{1,0:T(8,128)(2,1)}, bf16[128,2048]{1,0:T(8,128)(2,1)}, u32[]{:S(2)}, u32[]{:S(2)}) collective-permute-start(bf16[128,2048]{1,0:T(8,128)(2,1)} %get-tuple-element.137), channel_id=1, source_target_pairs={{0,8},{8,0},{16,24},{24,16},{1,9},{9,1},{17,25},{25,17},{2,10},{10... | collective-permute-start | bytes 1572872 | tf_op jit(solution)/shard_map/ppermute | solution.py:542
  522.8 30.9 %collective-permute-start.21 = (bf16[128,2048]{1,0:T(8,128)(2,1)}, bf16[128,2048]{1,0:T(8,128)(2,1)}, u32[]{:S(2)}, u32[]{:S(2)}) collective-permute-start(bf16[128,2048]{1,0:T(8,128)(2,1)} %get-tuple-element.136), channel_id=1, source_target_pairs={{0,16},{8,24},{16,0},{24,8},{1,17},{9,25},{17,1},{25,9},{2,18},{10... | collective-permute-start | bytes 1572872 | tf_op jit(solution)/shard_map/ppermute | solution.py:542
  535.4 11.5 %copy-start.21 = (bf16[1024,2048]{1,0:T(8,128)(2,1)S(1)}, bf16[1024,2048]{1,0:T(8,128)(2,1)}, u32[]{:S(2)}) copy-start(bf16[1024,2048]{1,0:T(8,128)(2,1)} %constant_dynamic-update-slice_fusion) | copy-start | bytes 12582916
  535.4 11.5 %copy-start.39 = (bf16[16,2048]{1,0:T(8,128)(2,1)S(1)}, bf16[16,2048]{1,0:T(8,128)(2,1)}, u32[]{:S(2)}) copy-start(bf16[16,2048]{1,0:T(8,128)(2,1)} %copy-done.38) | copy-start | bytes 196612
  535.4 11.5 %copy-start.50 = (f32[1024]{0:T(1024)S(1)}, f32[1024]{0:T(1024)}, u32[]{:S(2)}) copy-start(f32[1024]{0:T(1024)} %copy-done.49) | copy-start | bytes 12292
  550.4 5.5 collective-permute-start.29
  553.7 41.2 %collective-permute-start.25 = (bf16[128,2048]{1,0:T(8,128)(2,1)}, bf16[128,2048]{1,0:T(8,128)(2,1)}, u32[]{:S(2)}, u32[]{:S(2)}) collective-permute-start(bf16[128,2048]{1,0:T(8,128)(2,1)} %get-tuple-element.131), channel_id=1, source_target_pairs={{0,8},{8,0},{16,24},{24,16},{1,9},{9,1},{17,25},{25,17},{2,10},{10... | collective-permute-start | bytes 1572872 | tf_op jit(solution)/shard_map/ppermute | solution.py:542
  554.4 40.5 %collective-permute-start.26 = (bf16[128,2048]{1,0:T(8,128)(2,1)}, bf16[128,2048]{1,0:T(8,128)(2,1)}, u32[]{:S(2)}, u32[]{:S(2)}) collective-permute-start(bf16[128,2048]{1,0:T(8,128)(2,1)} %get-tuple-element.130), channel_id=1, source_target_pairs={{0,16},{8,24},{16,0},{24,8},{1,17},{9,25},{17,1},{25,9},{2,18},{10... | collective-permute-start | bytes 1572872 | tf_op jit(solution)/shard_map/ppermute | solution.py:542
  556.0 13.9 %collective-permute-start.30 = (f32[8,1352]{1,0:T(8,128)S(1)}, f32[8,1352]{1,0:T(8,128)S(1)}, u32[]{:S(2)}, u32[]{:S(2)}) collective-permute-start(f32[8,1352]{1,0:T(8,128)S(1)} %slice_select_fusion.1), channel_id=1, source_target_pairs={{0,8},{8,0},{16,24},{24,16},{1,9},{9,1},{17,25},{25,17},{2,10},{10... | collective-permute-start | bytes 129800 | tf_op jit(solution)/shard_map/ppermute | solution.py:577
  557.4 19.7 %copy-start.30 = (bf16[128,2048]{1,0:T(8,128)(2,1)S(1)}, bf16[128,2048]{1,0:T(8,128)(2,1)}, u32[]{:S(2)}) copy-start(bf16[128,2048]{1,0:T(8,128)(2,1)} %get-tuple-element.138) | copy-start | bytes 1572868
  559.8 20.3 %copy-start.29 = (bf16[128,2048]{1,0:T(8,128)(2,1)S(1)}, bf16[128,2048]{1,0:T(8,128)(2,1)}, u32[]{:S(2)}) copy-start(bf16[128,2048]{1,0:T(8,128)(2,1)} %get-tuple-element.135) | copy-start | bytes 1572868
  559.8 29.4 %collective-permute-start.39 = (bf16[64,2816]{1,0:T(8,128)(2,1)}, bf16[64,2816]{1,0:T(8,128)(2,1)}, u32[]{:S(2)}, u32[]{:S(2)}) collective-permute-start(bf16[64,2816]{1,0:T(8,128)(2,1)} %get-tuple-element.166), channel_id=1, source_target_pairs={{0,24},{8,16},{16,8},{24,0},{1,25},{9,17},{17,9},{25,1},{2,26},{10... | collective-permute-start | bytes 1081352 | tf_op jit(solution)/shard_map/ppermute | solution.py:542
  560.4 30.3 %collective-permute-start.38 = (bf16[64,2816]{1,0:T(8,128)(2,1)}, bf16[64,2816]{1,0:T(8,128)(2,1)}, u32[]{:S(2)}, u32[]{:S(2)}) collective-permute-start(bf16[64,2816]{1,0:T(8,128)(2,1)} %get-tuple-element.167), channel_id=1, source_target_pairs={{0,16},{8,24},{16,0},{24,8},{1,17},{9,25},{17,1},{25,9},{2,18},{10... | collective-permute-start | bytes 1081352 | tf_op jit(solution)/shard_map/ppermute | solution.py:542
  569.9 5.7 collective-permute-start.31
  575.7 4.3 collective-permute-start.32
  580.0 2.0 collective-permute-start.33
  582.0 11.5 %collective-permute-start.37 = (bf16[64,2816]{1,0:T(8,128)(2,1)}, bf16[64,2816]{1,0:T(8,128)(2,1)}, u32[]{:S(2)}, u32[]{:S(2)}) collective-permute-start(bf16[64,2816]{1,0:T(8,128)(2,1)} %get-tuple-element.168), channel_id=1, source_target_pairs={{0,8},{8,0},{16,24},{24,16},{1,9},{9,1},{17,25},{25,17},{2,10},{10... | collective-permute-start | bytes 1081352 | tf_op jit(solution)/shard_map/ppermute | solution.py:542
  589.2 26.6 %collective-permute-start.23 = (bf16[256,2048]{1,0:T(8,128)(2,1)S(1)}, bf16[256,2048]{1,0:T(8,128)(2,1)S(1)}, u32[]{:S(2)}, u32[]{:S(2)}) collective-permute-start(bf16[256,2048]{1,0:T(8,128)(2,1)S(1)} %pad_maximum_fusion.17), channel_id=1, source_target_pairs={{0,8},{8,0},{16,24},{24,16},{1,9},{9,1},{17,25},{25,17},{2,10},{10... | collective-permute-start | bytes 3145736 | tf_op jit(solution)/shard_map/ppermute | solution.py:542
  590.7 26.2 %collective-permute-start.24 = (bf16[256,2048]{1,0:T(8,128)(2,1)}, bf16[256,2048]{1,0:T(8,128)(2,1)S(1)}, u32[]{:S(2)}, u32[]{:S(2)}) collective-permute-start(bf16[256,2048]{1,0:T(8,128)(2,1)} %pad_maximum_fusion.18), channel_id=1, source_target_pairs={{0,16},{8,24},{16,0},{24,8},{1,17},{9,25},{17,1},{25,9},{2,18},{10... | collective-permute-start | bytes 3145736 | tf_op jit(solution)/shard_map/ppermute | solution.py:542
  596.9 41.0 %collective-permute-start.27 = (bf16[256,2048]{1,0:T(8,128)(2,1)S(1)}, bf16[256,2048]{1,0:T(8,128)(2,1)S(1)}, u32[]{:S(2)}, u32[]{:S(2)}) collective-permute-start(bf16[256,2048]{1,0:T(8,128)(2,1)S(1)} %pad_maximum_fusion.19), channel_id=1, source_target_pairs={{0,8},{8,0},{16,24},{24,16},{1,9},{9,1},{17,25},{25,17},{2,10},{10... | collective-permute-start | bytes 3145736 | tf_op jit(solution)/shard_map/ppermute | solution.py:542
  597.2 41.2 %collective-permute-start.28 = (bf16[256,2048]{1,0:T(8,128)(2,1)S(1)}, bf16[256,2048]{1,0:T(8,128)(2,1)S(1)}, u32[]{:S(2)}, u32[]{:S(2)}) collective-permute-start(bf16[256,2048]{1,0:T(8,128)(2,1)S(1)} %pad_maximum_fusion.20), channel_id=1, source_target_pairs={{0,16},{8,24},{16,0},{24,8},{1,17},{9,25},{17,1},{25,9},{2,18},{10... | collective-permute-start | bytes 3145736 | tf_op jit(solution)/shard_map/ppermute | solution.py:542
  615.9 22.5 %copy-start.31 = (bf16[256,2048]{1,0:T(8,128)(2,1)}, bf16[256,2048]{1,0:T(8,128)(2,1)S(1)}, u32[]{:S(2)}) copy-start(bf16[256,2048]{1,0:T(8,128)(2,1)S(1)} %collective-permute-done.23) | copy-start | bytes 3145732
  617.0 21.4 %copy-start.32 = (bf16[256,2048]{1,0:T(8,128)(2,1)}, bf16[256,2048]{1,0:T(8,128)(2,1)S(1)}, u32[]{:S(2)}) copy-start(bf16[256,2048]{1,0:T(8,128)(2,1)S(1)} %collective-permute-done.24) | copy-start | bytes 3145732
  652.4 10.2 %collective-permute-start.36 = (bf16[64,2048]{1,0:T(8,128)(2,1)S(1)}, bf16[64,2048]{1,0:T(8,128)(2,1)S(1)}, u32[]{:S(2)}, u32[]{:S(2)}) collective-permute-start(bf16[64,2048]{1,0:T(8,128)(2,1)S(1)} %get-tuple-element.182), channel_id=1, source_target_pairs={{0,24},{8,16},{16,8},{24,0},{1,25},{9,17},{17,9},{25,1},{2,26},{10... | collective-permute-start | bytes 786440 | tf_op jit(solution)/shard_map/ppermute | solution.py:542
  653.9 12.5 %collective-permute-start.35 = (bf16[64,2048]{1,0:T(8,128)(2,1)S(1)}, bf16[64,2048]{1,0:T(8,128)(2,1)S(1)}, u32[]{:S(2)}, u32[]{:S(2)}) collective-permute-start(bf16[64,2048]{1,0:T(8,128)(2,1)S(1)} %get-tuple-element.183), channel_id=1, source_target_pairs={{0,16},{8,24},{16,0},{24,8},{1,17},{9,25},{17,1},{25,9},{2,18},{10... | collective-permute-start | bytes 786440 | tf_op jit(solution)/shard_map/ppermute | solution.py:542
  654.4 12.1 %collective-permute-start.34 = (bf16[64,2048]{1,0:T(8,128)(2,1)S(1)}, bf16[64,2048]{1,0:T(8,128)(2,1)S(1)}, u32[]{:S(2)}, u32[]{:S(2)}) collective-permute-start(bf16[64,2048]{1,0:T(8,128)(2,1)S(1)} %get-tuple-element.184), channel_id=1, source_target_pairs={{0,8},{8,0},{16,24},{24,16},{1,9},{9,1},{17,25},{25,17},{2,10},{10... | collective-permute-start | bytes 786440 | tf_op jit(solution)/shard_map/ppermute | solution.py:542
  (50 other events, 174.7 us)
Sparse Core Ops, SparseCore 0:
  9.6 31.7 all-gather.4
  43.6 82.1 all-gather.6
  128.0 106.4 all-gather.8
  236.0 58.7 all-gather.10
  297.2 64.8 reduce-scatter.4
  365.6 102.2 reduce-scatter.6
  470.7 27.6 reduce-scatter.8
  517.1 90.8 reduce-scatter.10

commit v10 on v9

--- a/solution.py
+++ b/solution.py
@@ -551,22 +551,25 @@
     return jnp.concatenate([block, one, two, low, high], axis=0)
 
 
-def scattered(terms, ring, middle=(), end=()):
+def scattered(terms, ring, wait_first=None, wait_second=None):
     rows = terms.shape[0] // ring
     parts = [terms[by * rows : (by + 1) * rows] for by in range(ring)]
     total = parts[0].astype(F32)
     if ring != 4:
         for by in range(1, ring):
             total = total + swapped(parts[by], by, ring).astype(F32)
-        return total
+        return total if wait_first is None else (total, wait_first, wait_second)
     half = rows // 2
     low, high = swapped(parts[3][:half], 1, ring), swapped(parts[3][half:], 2, ring)
-    low, high = lax.optimization_barrier((low, high) + middle)[:2]
+    if wait_first is not None:
+        low, high, wait_first = lax.optimization_barrier((low, high, wait_first))
     two = jnp.concatenate([added(parts[2][:half], low), parts[2][half:]], axis=0)
     one = jnp.concatenate([parts[1][:half], added(parts[1][half:], high)], axis=0)
     one, two = swapped(one, 1, ring), swapped(two, 2, ring)
-    one, two = lax.optimization_barrier((one, two) + end)[:2]
-    return total + one.astype(F32) + two.astype(F32)
+    if wait_first is not None:
+        one, two, wait_second = lax.optimization_barrier((one, two, wait_second))
+    total = total + one.astype(F32) + two.astype(F32)
+    return total if wait_first is None else (total, wait_first, wait_second)
 
 
 def added(left, right):
@@ -855,19 +858,21 @@
 
     grad_gated = whole_head(dot_nt(grad_branch, w_output))
     term_output = core_sum(gated, grad_branch, lines)
-    output_share = line_sum(after(term_output, feed_sum), lines)
 
     slope = swish_sig * (1.0 + swish_pre * (1.0 - swish_sig))
     grad_swishpre = own_part((grad_gated * head_normed * slope).astype(BF16))
     grad_normed_head = grad_gated * swish_act
     term_head = jnp.sum(grad_normed_head * head_plain, axis=0) / copies
     scaled_head = grad_normed_head * gain_head
-    scaled_head = after(scaled_head, term_output)
     grad_mixed = head_factor * scaled_head - mixed * head_factor**3 * jnp.mean(
         scaled_head * mixed, axis=-1, keepdims=True
     )
+    result, grad_mixed, normed_late = scattered(
+        after(result_terms, grad_branch), ring, grad_mixed.astype(BF16), normed
+    )
+    layer_output = (hidden + result).astype(BF16).reshape(1, rows, width)
     grad_pre, grad_rate = mixer_backward(
-        order, ring, joined, grad_mixed.astype(BF16), rates, mask_rows, choice, starts
+        order, ring, joined, grad_mixed, rates, mask_rows, choice, starts
     )
     grad_logit = (grad_rate * jax.nn.sigmoid(-forget_logit) / TAU_GATE).astype(BF16)
     term_bias = jnp.sum(grad_logit.astype(F32), axis=1) / copies
@@ -878,11 +883,12 @@
             [own_part(grad_pre[:, at * head_size : (at + 1) * head_size]) for at in range(3)], axis=1
         )
     grad_pre = jnp.concatenate([grad_pre, grad_swishpre], axis=1)
-    term_pre = dot_tn(after(normed, output_share), grad_pre).astype(BF16)
-    pre_sum = lax.psum_scatter(term_pre, "batch", scatter_dimension=0, tiled=True)
+    term_pre = dot_tn(normed_late, grad_pre).astype(BF16)
+    pre_sum = lax.psum_scatter(
+        after(term_pre, feed_sum), "batch", scatter_dimension=0, tiled=True
+    )
+    output_share = line_sum(after(term_output, pre_sum), lines)
     grad_normed = dot_nt(after(grad_pre, term_pre), w_mixer) + dot_nn(grad_reduced, w_squeeze)
-    result = hidden + scattered(after(result_terms, grad_branch), ring, (term_pre,))
-    layer_output = result.astype(BF16).reshape(1, rows, width)
     grad_normed = dot_nt(after(grad_pre, term_pre), w_mixer) + dot_nn(grad_reduced, w_squeeze)
     term_mixer = restored(jnp.sum(grad_normed * plain_one, axis=0))
     term_squeeze = restored(dot_tn(grad_reduced, normed))

time: 692 us -> 658 us (0.951)
  waiting for transfers between devices: 143 us -> 121 us
  local copies, waits for them, and re-layouts: 92.8 us -> 84 us
    reduce_scatter x2, waiting for transfers between devices: 14.2 us -> 0.98 us  [line_sum(): lax.psum_scatter(terms, 'batch', scatter_dimension=0, axis_index_groups=g...]
    ppermute x12, waiting for transfers between devices: 41.1 us -> 33.6 us  [flipped(): lax.ppermute(block, axis, [(i, i ^ by) for i in range(lax.axis_size(axis))])]
    unnamed x162 -> x172, local copies, waits for them, and re-layouts: 39.9 us -> 39.3 us
  transfers between devices with their start and end apart: 48 -> 48, of which waited for: 28 -> 32; matrix products, arithmetic and copies ran while one was open for 34% -> 38% of each run, Pallas kernels for 29% -> 30%
where the time goes in v10:
time: 658 us; the launch traced here: 649 us
  Pallas kernels  195 us (30%)
  matrix products  147 us (22%)
  waiting for transfers between devices  121 us (18%)
  local copies, waits for them, and re-layouts  84 us (13%)
  starting transfers between devices  44.3 us (7%)
  other arithmetic  41.3 us (6%)
  between operations  16.2 us (2%)
    pallas_call x2, Pallas kernels, fold(): pl.pallas_call(functools.partial(fold_kernel, finish, len(given)), out_sh...  162 us
    ppermute x28, waiting for transfers between devices, swapped(): return lax.ppermute(block, 'seq', [(i, i ^ by) for i in range(ring)])  82.9 us
    dot_general x6, matrix products, dot_nt(): lax.dot_general(left, right, (((1,), (1,)), ((), ())), preferred_element_...  52.3 us
    dot_general x7, matrix products, dot_tn(): lax.dot_general(left, right, (((0,), (0,)), ((), ())), preferred_element_...  48.5 us
    dot_general x6, matrix products, dot_nn(): lax.dot_general(left, right, (((1,), (0,)), ((), ())), preferred_element_...  46.5 us
    unnamed x172, local copies, waits for them, and re-layouts  39.3 us
    ppermute x12, waiting for transfers between devices, flipped(): lax.ppermute(block, axis, [(i, i ^ by) for i in range(lax.axis_size(axis))])  33.6 us
    ppermute x28, starting transfers between devices, swapped(): return lax.ppermute(block, 'seq', [(i, i ^ by) for i in range(ring)])  32.1 us
  transfers between devices with their start and end apart: 48, of which 32 were waited for; matrix products, arithmetic and copies ran while one was open for 38% of the time, Pallas kernels for 30%

profile of v10, /device:TPU:0, one launch (start us, length us, event | category | flops | bytes accessed | tf_op | source)
XLA Modules:
  0.0 649.2 jit_solution(2827519089324272461)
XLA Ops:
  13.1 2.2 constant_dynamic-slice_fusion.26
  15.4 4.0 collective-permute-start.11
  20.5 6.0 collective-permute-done.11
  26.5 4.7 collective-permute-done.10
  34.2 3.0 constant_dynamic-slice_fusion.17
  37.2 1.8 collective-permute-start.18
  41.0 8.5 %collective-permute-done.18 = bf16[64,2816]{1,0:T(8,128)(2,1)S(1)} collective-permute-done((bf16[64,2816]{1,0:T(8,128)(2,1)S(1)}, bf16[64,2816]{1,0:T(8,128)(2,1)S(1)}, u32[]{:S(2)}, u32[]{:S(2)}) %collective-permute-start.18) | collective-permute-done | bytes 360480 | tf_op jit(solution)/shard_map/ppermute | solution.py:542
  49.5 6.6 %collective-permute-done.17 = bf16[64,2816]{1,0:T(8,128)(2,1)S(1)} collective-permute-done((bf16[64,2816]{1,0:T(8,128)(2,1)S(1)}, bf16[64,2816]{1,0:T(8,128)(2,1)S(1)}, u32[]{:S(2)}, u32[]{:S(2)}) %collective-permute-start.17) | collective-permute-done | bytes 360480 | tf_op jit(solution)/shard_map/ppermute | solution.py:542
  61.7 2.2 collective-permute-done.5
  64.0 2.5 collective-permute-start.6
  66.5 4.6 collective-permute-done.6
  79.7 19.1 %collective-permute-done.8 = bf16[16,1608]{1,0:T(8,128)(2,1)S(1)} collective-permute-done((bf16[16,1608]{1,0:T(8,128)(2,1)S(1)}, bf16[16,1608]{1,0:T(8,128)(2,1)S(1)}, u32[]{:S(2)}, u32[]{:S(2)}) %collective-permute-start.8) | collective-permute-done | bytes 51488 | tf_op jit(solution)/shard_map/ppermute | solution.py:580
  100.2 1.9 slice.208
  106.4 2.3 constant_dynamic-update-slice_fusion.3
  108.7 2.4 constant_dynamic-update-slice_fusion.2
  111.6 1.9 constant_dynamic-update-slice_fusion.1
  115.9 3.2 fusion.4
  123.5 2.3 all-gather.7.cloned.1.call-done
  128.7 12.5 %fusion.45 = (bf16[1024,2048]{1,0:T(8,128)(2,1)S(1)}, f32[1024,2048]{1,0:T(8,128)S(1)}) fusion(bf16[1024,2048]{1,0:T(8,128)(2,1)} %copy-done.19, bf16[2048,2048]{1,0:T(8,128)(2,1)} %all-gather.7.cloned.1.call-done), kind=kOutput, calls=%fused_computation.232 | convolution fusion | flops 8592031744 | bytes 25165824 | tf_op jit(solution)/shard_map/dot_general | solution.py:25
  141.2 11.9 %mixer_forward.1 = (f32[1024,512]{1,0:T(8,128)S(1)}, f32[128,1024]{1,0:T(8,128)S(1)}, f32[8,128,512]{2,1,0:T(8,128)S(1)}) custom-call(s32[1]{0:T(128)} %bitcast.mine, bf16[1024,2048]{1,0:T(8,128)(2,1)S(1)} %get-tuple-element.215.query.key.value, bf16[1024,2048]{1,0:T(8,128)(2,1)S(1)} %get-tuple-element.215.query.key.value, ...), custom_call_target="tpu_custom_call" | custom-call | flops 1048576000 | bytes 6291456 | tf_op jit(solution)/shard_map/mixer_forward/pallas_call | solution.py:285
  155.7 2.3 convolution_convert_fusion.5
  161.1 10.7 %collective-permute-done.14 = bf16[128,2048]{1,0:T(8,128)(2,1)S(1)} collective-permute-done((bf16[128,2048]{1,0:T(8,128)(2,1)S(1)}, bf16[128,2048]{1,0:T(8,128)(2,1)S(1)}, u32[]{:S(2)}, u32[]{:S(2)}) %collective-permute-start.14) | collective-permute-done | bytes 524320 | tf_op jit(solution)/shard_map/ppermute | solution.py:542
  171.8 1.7 collective-permute-done.15
  173.6 2.0 copy-done.46
  175.5 85.6 %fold_forward.1 = (bf16[4,256,2048]{2,1,0:T(8,128)(2,1)S(1)}, f32[256,2048]{1,0:T(8,128)S(1)}) custom-call(bf16[4,256,2048]{2,1,0:T(8,128)(2,1)S(1)} %bitcast.183, bf16[256,2048]{1,0:T(8,128)(2,1)S(1)} %bitcast.182, f32[1,2048]{1,0:T(1,128)S(1)} %reshape.412.refs_2_.refs_3_), custom_call_target="tpu_custom_call" | custom-call | tf_op jit(solution)/shard_map/fold_forward/pallas_call | solution.py:521
  262.5 2.1 copy-done.9
  264.6 17.3 %fusion.46 = f32[1024,2816]{1,0:T(8,128)S(1)} fusion(bf16[1024,2048]{1,0:T(8,128)(2,1)} %bitcast.185, bf16[2048,2816]{1,0:T(8,128)(2,1)} %all-gather.9.cloned.1.call-done), kind=kOutput, calls=%fused_computation.233 | convolution fusion | flops 11811160064 | bytes 27262976 | tf_op jit(solution)/shard_map/dot_general | solution.py:25
  281.9 1.8 multiply_convert_fusion.2
  283.8 3.5 copy-done.23
  288.9 8.1 %convolution_convert_fusion.1 = bf16[1408,2048]{1,0:T(8,128)(2,1)} fusion(bf16[1024,1408]{1,0:T(8,128)(2,1)S(1)} %multiply_convert_fusion.2, bf16[1024,2048]{1,0:T(8,128)(2,1)S(1)} %copy-done.47), kind=kOutput, calls=%fused_computation.9 | convolution fusion | flops 5908463616 | bytes 12845056 | tf_op jit(solution)/shard_map/dot_general | solution.py:33
  297.1 15.4 %multiply_convert_fusion.1 = (bf16[1024,1408]{1,0:T(8,128)(2,1)S(1)}, bf16[1024,1408]{1,0:T(8,128)(2,1)}) fusion(f32[1024,2816]{1,0:T(8,128)} %copy-done.23, bf16[1024,2048]{1,0:T(8,128)(2,1)} %copy-done.46, bf16[1408,2048]{1,0:T(8,128)(2,1)} %all-gather.11.cloned.1.call-done), kind=kOutput, calls=%fused_computation.12 | convolution fusion | flops 5924323328 | bytes 27262976 | tf_op jit(solution)/shard_map/dot_general | solution.py:29
  314.1 17.8 %convolution_convert_fusion.3 = bf16[1024,2048]{1,0:T(8,128)(2,1)} fusion(bf16[2048,2816]{1,0:T(8,128)(2,1)} %all-gather.9.cloned.1.call-done, bf16[1024,1408]{1,0:T(8,128)(2,1)} %get-tuple-element.117, bf16[1024,1408]{1,0:T(8,128)(2,1)S(1)} %get-tuple-element.116), kind=kOutput, calls=%fused_computation.19 | convolution fusion | flops 11824791552 | bytes 21495808 | tf_op jit(solution)/shard_map/dot_general | solution.py:29
  332.2 11.5 %convolution_convert_fusion.2 = bf16[1024,2816]{1,0:T(8,128)(2,1)} fusion(pred[]{:T(512)S(6)} %eq.86, bf16[1024,1408]{1,0:T(8,128)(2,1)} %get-tuple-element.117, bf16[1024,1408]{1,0:T(8,128)(2,1)} %copy-done.68, bf16[1024,256]{1,0:T(8,128)(2,1)S(1)} %get-tuple-element.134, bf16[1024,256]{1,0:T(8,128)(2,1)S(1)} %get-tuple-element.135, ...), kind=kOutput, calls=%fused_computation.16 | convolution fusion | flops 5937823744 | bytes 15728641 | tf_op jit(solution)/shard_map/dot_general | solution.py:33
  345.6 11.1 %convolution_convert_fusion.4 = bf16[1024,2048]{1,0:T(8,128)(2,1)} fusion(bf16[1024,1408]{1,0:T(8,128)(2,1)S(1)} %copy-done.27, bf16[1408,2048]{1,0:T(8,128)(2,1)} %all-gather.11.cloned.1.call-done), kind=kOutput, calls=%fused_computation.20 | convolution fusion | flops 5907677184 | bytes 12845056 | tf_op jit(solution)/shard_map/dot_general | solution.py:25
  356.7 8.6 %add_convert_fusion = bf16[1024,2816]{1,0:T(8,128)(2,1)} fusion(bf16[1024,2816]{1,0:T(8,128)(2,1)S(1)} %collective-permute-done.19, bf16[1024,1024]{1,0:T(8,128)(2,1)S(1)} %broadcast_select_fusion, bf16[1024,1408]{1,0:T(8,128)(2,1)S(1)} %copy-done.70, bf16[1024,1408]{1,0:T(8,128)(2,1)S(1)} %copy-done.69), kind=kOutput, calls=%fused_computation | convolution fusion | flops 5925765120 | bytes 19398656 | tf_op jit(solution)/shard_map/dot_general | solution.py:33
  367.2 2.2 copy-done.8
  369.4 76.7 %fold_backward.1 = (bf16[4,256,2048]{2,1,0:T(8,128)(2,1)S(1)}, f32[256,2048]{1,0:T(8,128)S(1)}, f32[1,2048]{1,0:T(1,128)S(1)}) custom-call(bf16[4,256,2048]{2,1,0:T(8,128)(2,1)S(1)} %bitcast.184, bf16[256,2048]{1,0:T(8,128)(2,1)} %bitcast.18.refs_1_, f32[256,2048]{1,0:T(8,128)S(1)} %copy-done.4, f32[1,2048]{1,0:T(1,128)S(1)} %reshape.412.refs_2_.refs_3_), custom_call_target="tpu_custom_call" | custom-call | tf_op jit(solution)/shard_map/fold_backward/pallas_call | solution.py:521
  449.2 5.2 multiply_reduce_fusion
  454.5 2.7 subtract_convert_fusion.grad_output
  457.2 2.5 collective-permute-done.20
  462.2 1.7 collective-permute-start.23
  464.4 21.2 %mixer_backward.1 = (bf16[1024,1536]{1,0:T(8,128)(2,1)S(1)}, f32[64,1024]{1,0:T(8,128)S(1)}) custom-call(s32[1]{0:T(128)} %bitcast.mine, bf16[1024,2048]{1,0:T(8,128)(2,1)S(1)} %copy-done.1, bf16[1024,2048]{1,0:T(8,128)(2,1)S(1)} %copy-done.1, bf16[1024,2048]{1,0:T(8,128)(2,1)S(1)} %copy-done.1, bf16[1024,512]{1,0:T(8,128)(2,1)S(1)} %subtract_convert_fusion.grad_output, ...), custom_call_target="tpu_custom_call" | custom-call | flops 2097152000 | bytes 10485760 | tf_op jit(solution)/shard_map/mixer_backward/pallas_call | solution.py:310
  487.3 11.9 %convolution_convert_fusion = bf16[2048,2048]{1,0:T(8,128)(2,1)} fusion(bf16[1024,2048]{1,0:T(8,128)(2,1)S(1)} %copy-done.20, bf16[1024,512]{1,0:T(8,128)(2,1)S(1)} %get-tuple-element.118, bf16[1024,1536]{1,0:T(8,128)(2,1)S(1)} %get-tuple-element.71), kind=kOutput, calls=%fused_computation.8 | convolution fusion | flops 8602517504 | bytes 16777216 | tf_op jit(solution)/shard_map/dot_general | solution.py:33
  502.7 4.6 convolution_convert_fusion.6
  511.6 2.9 fusion.48
  515.8 2.8 pad_maximum_fusion.1
  518.6 11.7 %fusion.47 = f32[1024,2048]{1,0:T(8,128)S(1)} fusion(bf16[1024,2048]{1,0:T(8,128)(2,1)S(1)} %pad_maximum_fusion.1, bf16[2048,2048]{1,0:T(8,128)(2,1)} %all-gather.7.cloned.1.call-done), kind=kOutput, calls=%fused_computation.234 | convolution fusion | flops 8589934592 | bytes 20971520 | tf_op jit(solution)/shard_map/dot_general | solution.py:29
  530.5 3.2 fusion.3
  535.9 2.7 collective-permute-done.28
  539.3 3.5 collective-permute-done.29
  542.8 2.5 collective-permute-start.30
  545.3 2.7 add_convert_fusion.1
  553.8 8.0 %collective-permute-done.24 = bf16[128,2048]{1,0:T(8,128)(2,1)S(1)} collective-permute-done((bf16[128,2048]{1,0:T(8,128)(2,1)S(1)}, bf16[128,2048]{1,0:T(8,128)(2,1)S(1)}, u32[]{:S(2)}, u32[]{:S(2)}) %collective-permute-start.24) | collective-permute-done | bytes 524320 | tf_op jit(solution)/shard_map/ppermute | solution.py:542
  571.5 15.9 %collective-permute-done.27 = bf16[256,2048]{1,0:T(8,128)(2,1)S(1)} collective-permute-done((bf16[256,2048]{1,0:T(8,128)(2,1)}, bf16[256,2048]{1,0:T(8,128)(2,1)S(1)}, u32[]{:S(2)}, u32[]{:S(2)}) %collective-permute-start.27) | collective-permute-done | bytes 1048608 | tf_op jit(solution)/shard_map/ppermute | solution.py:542
  588.6 3.1 convert_add_fusion
  591.7 1.9 copy.74
  595.1 3.1 copy.76
  603.7 4.9 fusion.17
  610.8 3.7 collective-permute-done.38
  622.5 3.7 collective-permute-done.35
  626.3 2.5 collective-permute-done.34
  629.5 2.4 reshape.416
  632.0 2.9 copy.117
  640.1 1.8 convert_element_type.366
  (387 shorter events, 115.3 us)
Async XLA Ops:
  7.2 108.7 %all-gather.5.cloned.1.call-start = ((), (), s32[]{:S(2)}) async-start(), calls=%async_computation.4 | async-start | bytes 2359296 | tf_op jit(solution)/shard_map/all_gather | solution.py:734
  7.9 117.9 %all-gather.7.cloned.1.call-start = ((), (), s32[]{:S(2)}) async-start(), calls=%async_computation.5 | async-start | bytes 9437184 | tf_op jit(solution)/shard_map/all_gather | solution.py:738
  15.4 11.1 %collective-permute-start.11 = (bf16[64,2048]{1,0:T(8,128)(2,1)S(1)}, bf16[64,2048]{1,0:T(8,128)(2,1)S(1)}, u32[]{:S(2)}, u32[]{:S(2)}) collective-permute-start(bf16[64,2048]{1,0:T(8,128)(2,1)S(1)} %bitcast.227), channel_id=1, source_target_pairs={{0,24},{8,16},{16,8},{24,0},{1,25},{9,17},{17,9},{25,1},{2,26},{10... | collective-permute-start | bytes 786440 | tf_op jit(solution)/shard_map/ppermute | solution.py:542
  19.5 11.8 %collective-permute-start.10 = (bf16[64,2048]{1,0:T(8,128)(2,1)S(1)}, bf16[64,2048]{1,0:T(8,128)(2,1)S(1)}, u32[]{:S(2)}, u32[]{:S(2)}) collective-permute-start(bf16[64,2048]{1,0:T(8,128)(2,1)S(1)} %bitcast.228), channel_id=1, source_target_pairs={{0,16},{8,24},{16,0},{24,8},{1,17},{9,25},{17,1},{25,9},{2,18},{10... | collective-permute-start | bytes 786440 | tf_op jit(solution)/shard_map/ppermute | solution.py:542
  20.2 11.3 %collective-permute-start.9 = (bf16[64,2048]{1,0:T(8,128)(2,1)S(1)}, bf16[64,2048]{1,0:T(8,128)(2,1)S(1)}, u32[]{:S(2)}, u32[]{:S(2)}) collective-permute-start(bf16[64,2048]{1,0:T(8,128)(2,1)S(1)} %bitcast.229), channel_id=1, source_target_pairs={{0,8},{8,0},{16,24},{24,16},{1,9},{9,1},{17,25},{25,17},{2,10},{10... | collective-permute-start | bytes 786440 | tf_op jit(solution)/shard_map/ppermute | solution.py:542
  33.0 231.6 %all-gather.9.cloned.1.call-start = ((), (), s32[]{:S(2)}) async-start(), calls=%async_computation.6 | async-start | bytes 12976128 | tf_op jit(solution)/shard_map/all_gather | solution.py:740
  37.2 12.3 %collective-permute-start.18 = (bf16[64,2816]{1,0:T(8,128)(2,1)S(1)}, bf16[64,2816]{1,0:T(8,128)(2,1)S(1)}, u32[]{:S(2)}, u32[]{:S(2)}) collective-permute-start(bf16[64,2816]{1,0:T(8,128)(2,1)S(1)} %bitcast.216), channel_id=1, source_target_pairs={{0,24},{8,16},{16,8},{24,0},{1,25},{9,17},{17,9},{25,1},{2,26},{10... | collective-permute-start | bytes 1081352 | tf_op jit(solution)/shard_map/ppermute | solution.py:542
  39.1 17.0 %collective-permute-start.17 = (bf16[64,2816]{1,0:T(8,128)(2,1)S(1)}, bf16[64,2816]{1,0:T(8,128)(2,1)S(1)}, u32[]{:S(2)}, u32[]{:S(2)}) collective-permute-start(bf16[64,2816]{1,0:T(8,128)(2,1)S(1)} %bitcast.217), channel_id=1, source_target_pairs={{0,16},{8,24},{16,0},{24,8},{1,17},{9,25},{17,1},{25,9},{2,18},{10... | collective-permute-start | bytes 1081352 | tf_op jit(solution)/shard_map/ppermute | solution.py:542
  40.4 16.0 %collective-permute-start.16 = (bf16[64,2816]{1,0:T(8,128)(2,1)S(1)}, bf16[64,2816]{1,0:T(8,128)(2,1)S(1)}, u32[]{:S(2)}, u32[]{:S(2)}) collective-permute-start(bf16[64,2816]{1,0:T(8,128)(2,1)S(1)} %bitcast.218), channel_id=1, source_target_pairs={{0,8},{8,0},{16,24},{24,16},{1,9},{9,1},{17,25},{25,17},{2,10},{10... | collective-permute-start | bytes 1081352 | tf_op jit(solution)/shard_map/ppermute | solution.py:542
  56.8 16.0 %copy-start.2 = (bf16[1,256,2048]{2,1,0:T(8,128)(2,1)S(1)}, bf16[1,256,2048]{2,1,0:T(8,128)(2,1)}, u32[]{:S(2)}) copy-start(bf16[1,256,2048]{2,1,0:T(8,128)(2,1)} %param.17) | copy-start | bytes 3145732
  58.1 239.0 %all-gather.11.cloned.1.call-start = ((), (), s32[]{:S(2)}) async-start(), calls=%async_computation.7 | async-start | bytes 6488064 | tf_op jit(solution)/shard_map/all_gather | solution.py:741
  58.9 1.2 collective-permute-start.4
  60.1 3.8 collective-permute-start.5
  64.0 7.1 %collective-permute-start.6 = (bf16[4,1608]{1,0:T(4,128)(2,1)S(1)}, bf16[4,1608]{1,0:T(4,128)(2,1)S(1)}, u32[]{:S(2)}, u32[]{:S(2)}) collective-permute-start(bf16[4,1608]{1,0:T(4,128)(2,1)S(1)} %pad_maximum_fusion.28), channel_id=1, source_target_pairs={{0,4},{1,5},{2,6},{3,7},{4,0},{5,1},{6,2},{7,3},{8,12},{9,13},{10,... | collective-permute-start | bytes 38600 | tf_op jit(solution)/shard_map/ppermute | solution.py:580
  71.2 6.8 %collective-permute-start.7 = (bf16[8,1608]{1,0:T(8,128)(2,1)S(1)}, bf16[8,1608]{1,0:T(8,128)(2,1)S(1)}, u32[]{:S(2)}, u32[]{:S(2)}) collective-permute-start(bf16[8,1608]{1,0:T(8,128)(2,1)S(1)} %pad_maximum_fusion.27), channel_id=1, source_target_pairs={{0,8},{8,0},{16,24},{24,16},{1,9},{9,1},{17,25},{25,17},{2,10},{10... | collective-permute-start | bytes 77192 | tf_op jit(solution)/shard_map/ppermute | solution.py:580
  75.9 28.9 %collective-permute-start = (bf16[256,2048]{1,0:T(8,128)(2,1)S(1)}, bf16[256,2048]{1,0:T(8,128)(2,1)}, u32[]{:S(2)}, u32[]{:S(2)}) collective-permute-start(bf16[256,2048]{1,0:T(8,128)(2,1)S(1)} %copy.67), channel_id=1, source_target_pairs={{0,8},{8,0},{16,24},{24,16},{1,9},{9,1},{17,25},{25,17},{2,10},{10... | collective-permute-start | bytes 3145736 | tf_op jit(solution)/shard_map/ppermute | solution.py:542
  76.5 23.7 %collective-permute-start.1 = (bf16[256,2048]{1,0:T(8,128)(2,1)S(1)}, bf16[256,2048]{1,0:T(8,128)(2,1)}, u32[]{:S(2)}, u32[]{:S(2)}) collective-permute-start(bf16[256,2048]{1,0:T(8,128)(2,1)S(1)} %copy.67), channel_id=1, source_target_pairs={{0,16},{8,24},{16,0},{24,8},{1,17},{9,25},{17,1},{25,9},{2,18},{10... | collective-permute-start | bytes 3145736 | tf_op jit(solution)/shard_map/ppermute | solution.py:542
  78.0 20.7 %collective-permute-start.8 = (bf16[16,1608]{1,0:T(8,128)(2,1)S(1)}, bf16[16,1608]{1,0:T(8,128)(2,1)S(1)}, u32[]{:S(2)}, u32[]{:S(2)}) collective-permute-start(bf16[16,1608]{1,0:T(8,128)(2,1)S(1)} %pad_maximum_fusion.26), channel_id=1, source_target_pairs={{0,16},{8,24},{16,0},{24,8},{1,17},{9,25},{17,1},{25,9},{2,18},{10... | collective-permute-start | bytes 154376 | tf_op jit(solution)/shard_map/ppermute | solution.py:580
  102.1 9.5 %collective-permute-start.2 = (bf16[128,2048]{1,0:T(8,128)(2,1)}, bf16[128,2048]{1,0:T(8,128)(2,1)}, u32[]{:S(2)}, u32[]{:S(2)}) collective-permute-start(bf16[128,2048]{1,0:T(8,128)(2,1)} %slice.208), channel_id=1, source_target_pairs={{0,8},{8,0},{16,24},{24,16},{1,9},{9,1},{17,25},{25,17},{2,10},{10... | collective-permute-start | bytes 1572872 | tf_op jit(solution)/shard_map/ppermute | solution.py:542
  104.4 16.0 %copy-start.40 = (bf16[16,2048]{1,0:T(8,128)(2,1)}, bf16[16,2048]{1,0:T(8,128)(2,1)S(1)}, u32[]{:S(2)}) copy-start(bf16[16,2048]{1,0:T(8,128)(2,1)S(1)} %reshape.381) | copy-start | bytes 196612
  104.5 17.1 %copy-start.51 = (bf16[256,16]{1,0:T(8,128)(2,1)}, bf16[256,16]{1,0:T(8,128)(2,1)S(1)}, u32[]{:S(2)}) copy-start(bf16[256,16]{1,0:T(8,128)(2,1)S(1)} %reshape.378) | copy-start | bytes 24580
  104.7 260.7 %reduce-scatter.5.cloned.1.call-start = ((), (), s32[]{:S(2)}) async-start(), calls=%async_computation.8 | async-start | bytes 6488064 | tf_op jit(solution)/shard_map/reduce_scatter | solution.py:833
  105.8 9.2 %collective-permute-start.3 = (bf16[128,2048]{1,0:T(8,128)(2,1)S(1)}, bf16[128,2048]{1,0:T(8,128)(2,1)S(1)}, u32[]{:S(2)}, u32[]{:S(2)}) collective-permute-start(bf16[128,2048]{1,0:T(8,128)(2,1)S(1)} %slice.209), channel_id=1, source_target_pairs={{0,16},{8,24},{16,0},{24,8},{1,17},{9,25},{17,1},{25,9},{2,18},{10... | collective-permute-start | bytes 1572872 | tf_op jit(solution)/shard_map/ppermute | solution.py:542
  125.8 15.4 %copy-start.6 = (f32[128,1024]{1,0:T(8,128)S(1)}, f32[128,1024]{1,0:T(8,128)}, u32[]{:S(2)}) copy-start(f32[128,1024]{1,0:T(8,128)} %pad_maximum_fusion.22.rate) | copy-start | bytes 1572868
  125.8 34.4 %collective-permute-start.12 = (bf16[256,2048]{1,0:T(8,128)(2,1)}, bf16[256,2048]{1,0:T(8,128)(2,1)S(1)}, u32[]{:S(2)}, u32[]{:S(2)}) collective-permute-start(bf16[256,2048]{1,0:T(8,128)(2,1)} %bitcast.18.refs_1_), channel_id=1, source_target_pairs={{0,8},{8,0},{16,24},{24,16},{1,9},{9,1},{17,25},{25,17},{2,10},{10... | collective-permute-start | bytes 3145736 | tf_op jit(solution)/shard_map/ppermute | solution.py:542
  127.3 30.8 %collective-permute-start.13 = (bf16[256,2048]{1,0:T(8,128)(2,1)}, bf16[256,2048]{1,0:T(8,128)(2,1)S(1)}, u32[]{:S(2)}, u32[]{:S(2)}) collective-permute-start(bf16[256,2048]{1,0:T(8,128)(2,1)} %bitcast.18.refs_1_), channel_id=1, source_target_pairs={{0,16},{8,24},{16,0},{24,8},{1,17},{9,25},{17,1},{25,9},{2,18},{10... | collective-permute-start | bytes 3145736 | tf_op jit(solution)/shard_map/ppermute | solution.py:542
  141.2 12.0 %copy-start = (bf16[1024,2048]{1,0:T(8,128)(2,1)}, bf16[1024,2048]{1,0:T(8,128)(2,1)S(1)}, u32[]{:S(2)}) copy-start(bf16[1024,2048]{1,0:T(8,128)(2,1)S(1)} %get-tuple-element.215.query.key.value) | copy-start | bytes 12582916
  141.2 12.2 %copy-start.31 = (f32[1024,2048]{1,0:T(8,128)}, f32[1024,2048]{1,0:T(8,128)S(1)}, u32[]{:S(2)}) copy-start(f32[1024,2048]{1,0:T(8,128)S(1)} %get-tuple-element.216) | copy-start | bytes 25165828
  158.1 13.6 %collective-permute-start.14 = (bf16[128,2048]{1,0:T(8,128)(2,1)S(1)}, bf16[128,2048]{1,0:T(8,128)(2,1)S(1)}, u32[]{:S(2)}, u32[]{:S(2)}) collective-permute-start(bf16[128,2048]{1,0:T(8,128)(2,1)S(1)} %slice.212), channel_id=1, source_target_pairs={{0,8},{8,0},{16,24},{24,16},{1,9},{9,1},{17,25},{25,17},{2,10},{10... | collective-permute-start | bytes 1572872 | tf_op jit(solution)/shard_map/ppermute | solution.py:542
  160.2 13.3 %collective-permute-start.15 = (bf16[128,2048]{1,0:T(8,128)(2,1)S(1)}, bf16[128,2048]{1,0:T(8,128)(2,1)S(1)}, u32[]{:S(2)}, u32[]{:S(2)}) collective-permute-start(bf16[128,2048]{1,0:T(8,128)(2,1)S(1)} %slice.213), channel_id=1, source_target_pairs={{0,16},{8,24},{16,0},{24,8},{1,17},{9,25},{17,1},{25,9},{2,18},{10... | collective-permute-start | bytes 1572872 | tf_op jit(solution)/shard_map/ppermute | solution.py:542
  297.0 202.1 %reduce-scatter.7.cloned.1.call-start = ((), (), s32[]{:S(2)}) async-start(), calls=%async_computation.9 | async-start | bytes 7208960 | tf_op jit(solution)/shard_map/reduce_scatter | solution.py:633
  314.1 17.8 %copy-start.10 = (bf16[4,256,2048]{2,1,0:T(8,128)(2,1)S(1)}, bf16[4,256,2048]{2,1,0:T(8,128)(2,1)}, u32[]{:S(2)}) copy-start(bf16[4,256,2048]{2,1,0:T(8,128)(2,1)} %copy-done.9) | copy-start | bytes 12582916
  343.8 12.9 %collective-permute-start.19 = (bf16[1024,2816]{1,0:T(8,128)(2,1)}, bf16[1024,2816]{1,0:T(8,128)(2,1)S(1)}, u32[]{:S(2)}, u32[]{:S(2)}) collective-permute-start(bf16[1024,2816]{1,0:T(8,128)(2,1)} %convolution_convert_fusion.2), channel_id=1, source_target_pairs={{0,1},{1,0},{2,3},{3,2},{4,5},{5,4},{6,7},{7,6},{8,9},{9,8},{10,11... | collective-permute-start | bytes 17301512 | tf_op jit(solution)/shard_map/ppermute | solution.py:580
  345.6 11.1 %copy-start.69 = (bf16[1024,1408]{1,0:T(8,128)(2,1)S(1)}, bf16[1024,1408]{1,0:T(8,128)(2,1)}, u32[]{:S(2)}) copy-start(bf16[1024,1408]{1,0:T(8,128)(2,1)} %copy-done.68) | copy-start | bytes 8650756
  345.6 11.1 %copy-start.70 = (bf16[1024,1408]{1,0:T(8,128)(2,1)S(1)}, bf16[1024,1408]{1,0:T(8,128)(2,1)}, u32[]{:S(2)}) copy-start(bf16[1024,1408]{1,0:T(8,128)(2,1)} %get-tuple-element.117) | copy-start | bytes 8650756
  365.4 249.6 %reduce-scatter.9.cloned.1.call-start = ((), (), s32[]{:S(2)}) async-start(), calls=%async_computation.10 | async-start | bytes 9437184 | tf_op jit(solution)/shard_map/reduce_scatter | solution.py:887
  369.4 76.7 %copy-start.25 = (bf16[1024,2048]{1,0:T(8,128)(2,1)S(1)}, bf16[1024,2048]{1,0:T(8,128)(2,1)}, u32[]{:S(2)}) copy-start(bf16[1024,2048]{1,0:T(8,128)(2,1)} %convolution_convert_fusion.4) | copy-start | bytes 12582916
  446.3 13.4 %collective-permute-start.20 = (bf16[128,2048]{1,0:T(8,128)(2,1)S(1)}, bf16[128,2048]{1,0:T(8,128)(2,1)S(1)}, u32[]{:S(2)}, u32[]{:S(2)}) collective-permute-start(bf16[128,2048]{1,0:T(8,128)(2,1)S(1)} %get-tuple-element.131), channel_id=1, source_target_pairs={{0,8},{8,0},{16,24},{24,16},{1,9},{9,1},{17,25},{25,17},{2,10},{10... | collective-permute-start | bytes 1572872 | tf_op jit(solution)/shard_map/ppermute | solution.py:542
  447.9 13.3 %collective-permute-start.21 = (bf16[128,2048]{1,0:T(8,128)(2,1)S(1)}, bf16[128,2048]{1,0:T(8,128)(2,1)S(1)}, u32[]{:S(2)}, u32[]{:S(2)}) collective-permute-start(bf16[128,2048]{1,0:T(8,128)(2,1)S(1)} %get-tuple-element.130), channel_id=1, source_target_pairs={{0,16},{8,24},{16,0},{24,8},{1,17},{9,25},{17,1},{25,9},{2,18},{10... | collective-permute-start | bytes 1572872 | tf_op jit(solution)/shard_map/ppermute | solution.py:542
  454.5 31.6 %copy-start.36 = (bf16[1024,512]{1,0:T(8,128)(2,1)}, bf16[1024,512]{1,0:T(8,128)(2,1)S(1)}, u32[]{:S(2)}) copy-start(bf16[1024,512]{1,0:T(8,128)(2,1)S(1)} %get-tuple-element.118) | copy-start | bytes 3145732
  461.7 24.0 %collective-permute-start.22 = (bf16[256,2048]{1,0:T(8,128)(2,1)S(1)}, bf16[256,2048]{1,0:T(8,128)(2,1)}, u32[]{:S(2)}, u32[]{:S(2)}) collective-permute-start(bf16[256,2048]{1,0:T(8,128)(2,1)S(1)} %pad_maximum_fusion.15), channel_id=1, source_target_pairs={{0,8},{8,0},{16,24},{24,16},{1,9},{9,1},{17,25},{25,17},{2,10},{10... | collective-permute-start | bytes 3145736 | tf_op jit(solution)/shard_map/ppermute | solution.py:542
  462.2 23.9 %collective-permute-start.23 = (bf16[256,2048]{1,0:T(8,128)(2,1)S(1)}, bf16[256,2048]{1,0:T(8,128)(2,1)}, u32[]{:S(2)}, u32[]{:S(2)}) collective-permute-start(bf16[256,2048]{1,0:T(8,128)(2,1)S(1)} %pad_maximum_fusion.16), channel_id=1, source_target_pairs={{0,16},{8,24},{16,0},{24,8},{1,17},{9,25},{17,1},{25,9},{2,18},{10... | collective-permute-start | bytes 3145736 | tf_op jit(solution)/shard_map/ppermute | solution.py:542
  464.4 22.9 %copy-start.20 = (bf16[1024,2048]{1,0:T(8,128)(2,1)S(1)}, bf16[1024,2048]{1,0:T(8,128)(2,1)}, u32[]{:S(2)}) copy-start(bf16[1024,2048]{1,0:T(8,128)(2,1)} %copy-done.19) | copy-start | bytes 12582916
  499.2 140.9 %reduce-scatter.11.cloned.1.call-start = ((), (), s32[]{:S(2)}) async-start(), calls=%async_computation.11 | async-start | bytes 1310720 | tf_op jit(solution)/shard_map/reduce_scatter | solution.py:633
  518.6 11.8 %copy-start.22 = (bf16[1024,2048]{1,0:T(8,128)(2,1)S(1)}, bf16[1024,2048]{1,0:T(8,128)(2,1)}, u32[]{:S(2)}) copy-start(bf16[1024,2048]{1,0:T(8,128)(2,1)} %constant_dynamic-update-slice_fusion) | copy-start | bytes 12582916
  518.6 11.8 %copy-start.41 = (bf16[16,2048]{1,0:T(8,128)(2,1)S(1)}, bf16[16,2048]{1,0:T(8,128)(2,1)}, u32[]{:S(2)}) copy-start(bf16[16,2048]{1,0:T(8,128)(2,1)} %copy-done.40) | copy-start | bytes 196612
  518.6 11.8 %copy-start.43 = (bf16[1024,16]{0,1:T(8,128)(2,1)S(1)}, bf16[1024,16]{0,1:T(8,128)(2,1)}, u32[]{:S(2)}) copy-start(bf16[1024,16]{0,1:T(8,128)(2,1)} %copy-done.42) | copy-start | bytes 98308
  518.6 11.8 %copy-start.57 = (f32[1024]{0:T(1024)S(1)}, f32[1024]{0:T(1024)}, u32[]{:S(2)}) copy-start(f32[1024]{0:T(1024)} %copy-done.56) | copy-start | bytes 12292
  534.0 4.6 collective-permute-start.28
  535.9 9.4 %collective-permute-start.36 = (bf16[256,2048]{1,0:T(8,128)(2,1)}, bf16[256,2048]{1,0:T(8,128)(2,1)}, u32[]{:S(2)}, u32[]{:S(2)}) collective-permute-start(bf16[256,2048]{1,0:T(8,128)(2,1)} %broadcast_select_fusion.1), channel_id=1, source_target_pairs={{0,1},{1,0},{2,3},{3,2},{4,5},{5,4},{6,7},{7,6},{8,9},{9,8},{10,11... | collective-permute-start | bytes 3145736 | tf_op jit(solution)/shard_map/ppermute | solution.py:580
  538.6 4.1 collective-permute-start.29
  542.8 5.7 collective-permute-start.30
  548.5 5.2 collective-permute-start.31
  551.5 10.2 %collective-permute-start.24 = (bf16[128,2048]{1,0:T(8,128)(2,1)S(1)}, bf16[128,2048]{1,0:T(8,128)(2,1)S(1)}, u32[]{:S(2)}, u32[]{:S(2)}) collective-permute-start(bf16[128,2048]{1,0:T(8,128)(2,1)S(1)} %get-tuple-element.124), channel_id=1, source_target_pairs={{0,16},{8,24},{16,0},{24,8},{1,17},{9,25},{17,1},{25,9},{2,18},{10... | collective-permute-start | bytes 1572872 | tf_op jit(solution)/shard_map/ppermute | solution.py:542
  552.0 11.0 %collective-permute-start.26 = (bf16[128,2048]{1,0:T(8,128)(2,1)S(1)}, bf16[128,2048]{1,0:T(8,128)(2,1)S(1)}, u32[]{:S(2)}, u32[]{:S(2)}) collective-permute-start(bf16[128,2048]{1,0:T(8,128)(2,1)S(1)} %get-tuple-element.123), channel_id=1, source_target_pairs={{0,8},{8,0},{16,24},{24,16},{1,9},{9,1},{17,25},{25,17},{2,10},{10... | collective-permute-start | bytes 1572872 | tf_op jit(solution)/shard_map/ppermute | solution.py:542
  553.7 15.0 %collective-permute-start.32 = (f32[1,1352]{1,0:T(1,128)S(1)}, f32[1,1352]{1,0:T(1,128)S(1)}, u32[]{:S(2)}, u32[]{:S(2)}) collective-permute-start(f32[1,1352]{1,0:T(1,128)S(1)} %broadcast_select_fusion.13), channel_id=1, source_target_pairs={{0,1},{1,0},{2,3},{3,2},{4,5},{5,4},{6,7},{7,6},{8,9},{9,8},{10,11... | collective-permute-start | bytes 16232 | tf_op jit(solution)/shard_map/ppermute | solution.py:580
  565.6 21.7 %collective-permute-start.27 = (bf16[256,2048]{1,0:T(8,128)(2,1)}, bf16[256,2048]{1,0:T(8,128)(2,1)S(1)}, u32[]{:S(2)}, u32[]{:S(2)}) collective-permute-start(bf16[256,2048]{1,0:T(8,128)(2,1)} %pad_maximum_fusion.18), channel_id=1, source_target_pairs={{0,16},{8,24},{16,0},{24,8},{1,17},{9,25},{17,1},{25,9},{2,18},{10... | collective-permute-start | bytes 3145736 | tf_op jit(solution)/shard_map/ppermute | solution.py:542
  567.2 21.4 %collective-permute-start.25 = (bf16[256,2048]{1,0:T(8,128)(2,1)}, bf16[256,2048]{1,0:T(8,128)(2,1)S(1)}, u32[]{:S(2)}, u32[]{:S(2)}) collective-permute-start(bf16[256,2048]{1,0:T(8,128)(2,1)} %pad_maximum_fusion.17), channel_id=1, source_target_pairs={{0,8},{8,0},{16,24},{24,16},{1,9},{9,1},{17,25},{25,17},{2,10},{10... | collective-permute-start | bytes 3145736 | tf_op jit(solution)/shard_map/ppermute | solution.py:542
  600.2 10.7 %collective-permute-start.39 = (bf16[64,2816]{1,0:T(8,128)(2,1)S(1)}, bf16[64,2816]{1,0:T(8,128)(2,1)S(1)}, u32[]{:S(2)}, u32[]{:S(2)}) collective-permute-start(bf16[64,2816]{1,0:T(8,128)(2,1)S(1)} %get-tuple-element.160), channel_id=1, source_target_pairs={{0,24},{8,16},{16,8},{24,0},{1,25},{9,17},{17,9},{25,1},{2,26},{10... | collective-permute-start | bytes 1081352 | tf_op jit(solution)/shard_map/ppermute | solution.py:542
  601.6 12.9 %collective-permute-start.38 = (bf16[64,2816]{1,0:T(8,128)(2,1)S(1)}, bf16[64,2816]{1,0:T(8,128)(2,1)S(1)}, u32[]{:S(2)}, u32[]{:S(2)}) collective-permute-start(bf16[64,2816]{1,0:T(8,128)(2,1)S(1)} %get-tuple-element.161), channel_id=1, source_target_pairs={{0,16},{8,24},{16,0},{24,8},{1,17},{9,25},{17,1},{25,9},{2,18},{10... | collective-permute-start | bytes 1081352 | tf_op jit(solution)/shard_map/ppermute | solution.py:542
  603.1 11.6 %collective-permute-start.37 = (bf16[64,2816]{1,0:T(8,128)(2,1)S(1)}, bf16[64,2816]{1,0:T(8,128)(2,1)S(1)}, u32[]{:S(2)}, u32[]{:S(2)}) collective-permute-start(bf16[64,2816]{1,0:T(8,128)(2,1)S(1)} %get-tuple-element.162), channel_id=1, source_target_pairs={{0,8},{8,0},{16,24},{24,16},{1,9},{9,1},{17,25},{25,17},{2,10},{10... | collective-permute-start | bytes 1081352 | tf_op jit(solution)/shard_map/ppermute | solution.py:542
  616.3 10.0 %collective-permute-start.35 = (bf16[64,2048]{1,0:T(8,128)(2,1)S(1)}, bf16[64,2048]{1,0:T(8,128)(2,1)S(1)}, u32[]{:S(2)}, u32[]{:S(2)}) collective-permute-start(bf16[64,2048]{1,0:T(8,128)(2,1)S(1)} %get-tuple-element.176), channel_id=1, source_target_pairs={{0,24},{8,16},{16,8},{24,0},{1,25},{9,17},{17,9},{25,1},{2,26},{10... | collective-permute-start | bytes 786440 | tf_op jit(solution)/shard_map/ppermute | solution.py:542
  617.7 11.1 %collective-permute-start.34 = (bf16[64,2048]{1,0:T(8,128)(2,1)S(1)}, bf16[64,2048]{1,0:T(8,128)(2,1)S(1)}, u32[]{:S(2)}, u32[]{:S(2)}) collective-permute-start(bf16[64,2048]{1,0:T(8,128)(2,1)S(1)} %get-tuple-element.177), channel_id=1, source_target_pairs={{0,16},{8,24},{16,0},{24,8},{1,17},{9,25},{17,1},{25,9},{2,18},{10... | collective-permute-start | bytes 786440 | tf_op jit(solution)/shard_map/ppermute | solution.py:542
  619.0 10.1 %collective-permute-start.33 = (bf16[64,2048]{1,0:T(8,128)(2,1)S(1)}, bf16[64,2048]{1,0:T(8,128)(2,1)S(1)}, u32[]{:S(2)}, u32[]{:S(2)}) collective-permute-start(bf16[64,2048]{1,0:T(8,128)(2,1)S(1)} %get-tuple-element.178), channel_id=1, source_target_pairs={{0,8},{8,0},{16,24},{24,16},{1,9},{9,1},{17,25},{25,17},{2,10},{10... | collective-permute-start | bytes 786440 | tf_op jit(solution)/shard_map/ppermute | solution.py:542
  (55 other events, 164.5 us)
Sparse Core Ops, SparseCore 0:
  9.6 31.7 all-gather.4
  43.6 82.1 all-gather.6
  128.0 106.4 all-gather.8
  236.0 58.7 all-gather.10
  297.2 64.8 reduce-scatter.4
  365.5 102.1 reduce-scatter.6
  499.3 90.3 reduce-scatter.8
  615.1 24.9 reduce-scatter.10

commit v11 on v10

--- a/solution.py
+++ b/solution.py
@@ -857,7 +857,6 @@
         grad_branch = gathered(grad_hidden.astype(BF16), ring)
 
     grad_gated = whole_head(dot_nt(grad_branch, w_output))
-    term_output = core_sum(gated, grad_branch, lines)
 
     slope = swish_sig * (1.0 + swish_pre * (1.0 - swish_sig))
     grad_swishpre = own_part((grad_gated * head_normed * slope).astype(BF16))
@@ -871,6 +870,9 @@
         after(result_terms, grad_branch), ring, grad_mixed.astype(BF16), normed
     )
     layer_output = (hidden + result).astype(BF16).reshape(1, rows, width)
+    term_output = core_sum(after(gated, grad_mixed), grad_branch, lines)
+    output_share = line_sum(after(term_output, feed_sum), lines)
+    grad_mixed = after(grad_mixed, term_output)
     grad_pre, grad_rate = mixer_backward(
         order, ring, joined, grad_mixed, rates, mask_rows, choice, starts
     )
@@ -885,9 +887,8 @@
     grad_pre = jnp.concatenate([grad_pre, grad_swishpre], axis=1)
     term_pre = dot_tn(normed_late, grad_pre).astype(BF16)
     pre_sum = lax.psum_scatter(
-        after(term_pre, feed_sum), "batch", scatter_dimension=0, tiled=True
-    )
-    output_share = line_sum(after(term_output, pre_sum), lines)
+        after(term_pre, output_share), "batch", scatter_dimension=0, tiled=True
+    )
     grad_normed = dot_nt(after(grad_pre, term_pre), w_mixer) + dot_nn(grad_reduced, w_squeeze)
     grad_normed = dot_nt(after(grad_pre, term_pre), w_mixer) + dot_nn(grad_reduced, w_squeeze)
     term_mixer = restored(jnp.sum(grad_normed * plain_one, axis=0))

time: 658 us -> 657 us (level)
    unnamed x172 -> x154, local copies, waits for them, and re-layouts: 39.3 us -> 42.4 us
  transfers between devices with their start and end apart: 48 -> 48, of which waited for: 32 -> 30; matrix products, arithmetic and copies ran while one was open for 38% -> 36% of each run, Pallas kernels for 30% -> 30%
where the time goes in v11:
time: 657 us; the launch traced here: 648 us
  Pallas kernels  198 us (30%)
  matrix products  146 us (22%)
  waiting for transfers between devices  121 us (18%)
  local copies, waits for them, and re-layouts  85.4 us (13%)
  starting transfers between devices  42.8 us (7%)
  other arithmetic  39.9 us (6%)
  between operations  16.1 us (2%)
    pallas_call x2, Pallas kernels, fold(): pl.pallas_call(functools.partial(fold_kernel, finish, len(given)), out_sh...  164 us
    ppermute x28, waiting for transfers between devices, swapped(): return lax.ppermute(block, 'seq', [(i, i ^ by) for i in range(ring)])  81.2 us
    dot_general x6, matrix products, dot_nt(): lax.dot_general(left, right, (((1,), (1,)), ((), ())), preferred_element_...  53.1 us
    dot_general x6, matrix products, dot_nn(): lax.dot_general(left, right, (((1,), (0,)), ((), ())), preferred_element_...  46.5 us
    dot_general x7, matrix products, dot_tn(): lax.dot_general(left, right, (((0,), (0,)), ((), ())), preferred_element_...  46 us
    unnamed x154, local copies, waits for them, and re-layouts  42.4 us
    ppermute x12, waiting for transfers between devices, flipped(): lax.ppermute(block, axis, [(i, i ^ by) for i in range(lax.axis_size(axis))])  38.4 us
    ppermute x28, starting transfers between devices, swapped(): return lax.ppermute(block, 'seq', [(i, i ^ by) for i in range(ring)])  31.2 us
  transfers between devices with their start and end apart: 48, of which 30 were waited for; matrix products, arithmetic and copies ran while one was open for 36% of the time, Pallas kernels for 30%

profile of v11, /device:TPU:0, one launch (start us, length us, event | category | flops | bytes accessed | tf_op | source)
XLA Modules:
  0.0 648.1 jit_solution(14355452852852775452)
XLA Ops:
  13.1 2.2 constant_dynamic-slice_fusion.26
  15.4 4.0 collective-permute-start.11
  20.5 6.0 collective-permute-done.11
  26.5 4.7 collective-permute-done.10
  34.2 3.0 constant_dynamic-slice_fusion.17
  37.2 1.8 collective-permute-start.18
  41.0 8.5 %collective-permute-done.18 = bf16[64,2816]{1,0:T(8,128)(2,1)S(1)} collective-permute-done((bf16[64,2816]{1,0:T(8,128)(2,1)S(1)}, bf16[64,2816]{1,0:T(8,128)(2,1)S(1)}, u32[]{:S(2)}, u32[]{:S(2)}) %collective-permute-start.18) | collective-permute-done | bytes 360480 | tf_op jit(solution)/shard_map/ppermute | solution.py:542
  49.5 6.6 %collective-permute-done.17 = bf16[64,2816]{1,0:T(8,128)(2,1)S(1)} collective-permute-done((bf16[64,2816]{1,0:T(8,128)(2,1)S(1)}, bf16[64,2816]{1,0:T(8,128)(2,1)S(1)}, u32[]{:S(2)}, u32[]{:S(2)}) %collective-permute-start.17) | collective-permute-done | bytes 360480 | tf_op jit(solution)/shard_map/ppermute | solution.py:542
  61.7 2.2 collective-permute-done.5
  64.0 2.5 collective-permute-start.6
  66.5 4.6 collective-permute-done.6
  79.7 19.1 %collective-permute-done.8 = bf16[16,1608]{1,0:T(8,128)(2,1)S(1)} collective-permute-done((bf16[16,1608]{1,0:T(8,128)(2,1)S(1)}, bf16[16,1608]{1,0:T(8,128)(2,1)S(1)}, u32[]{:S(2)}, u32[]{:S(2)}) %collective-permute-start.8) | collective-permute-done | bytes 51488 | tf_op jit(solution)/shard_map/ppermute | solution.py:580
  100.2 1.9 slice.208
  106.4 2.3 constant_dynamic-update-slice_fusion.3
  108.7 2.4 constant_dynamic-update-slice_fusion.2
  111.6 1.9 constant_dynamic-update-slice_fusion.1
  115.9 3.2 fusion.4
  120.4 2.0 copy-done.19
  128.7 12.5 %fusion.45 = (bf16[1024,2048]{1,0:T(8,128)(2,1)S(1)}, f32[1024,2048]{1,0:T(8,128)S(1)}) fusion(bf16[1024,2048]{1,0:T(8,128)(2,1)} %copy-done.19, bf16[2048,2048]{1,0:T(8,128)(2,1)} %all-gather.7.cloned.1.call-done), kind=kOutput, calls=%fused_computation.232 | convolution fusion | flops 8592031744 | bytes 25165824 | tf_op jit(solution)/shard_map/dot_general | solution.py:25
  141.2 11.9 %mixer_forward.1 = (f32[1024,512]{1,0:T(8,128)S(1)}, f32[128,1024]{1,0:T(8,128)S(1)}, f32[8,128,512]{2,1,0:T(8,128)S(1)}) custom-call(s32[1]{0:T(128)} %bitcast.mine, bf16[1024,2048]{1,0:T(8,128)(2,1)S(1)} %get-tuple-element.219.query.key.value, bf16[1024,2048]{1,0:T(8,128)(2,1)S(1)} %get-tuple-element.219.query.key.value, ...), custom_call_target="tpu_custom_call" | custom-call | flops 1048576000 | bytes 6291456 | tf_op jit(solution)/shard_map/mixer_forward/pallas_call | solution.py:285
  155.7 2.3 convolution_convert_fusion.5
  161.1 10.7 %collective-permute-done.14 = bf16[128,2048]{1,0:T(8,128)(2,1)S(1)} collective-permute-done((bf16[128,2048]{1,0:T(8,128)(2,1)S(1)}, bf16[128,2048]{1,0:T(8,128)(2,1)S(1)}, u32[]{:S(2)}, u32[]{:S(2)}) %collective-permute-start.14) | collective-permute-done | bytes 524320 | tf_op jit(solution)/shard_map/ppermute | solution.py:542
  173.6 2.0 copy-done.42
  175.6 87.6 %fold_forward.1 = (bf16[4,256,2048]{2,1,0:T(8,128)(2,1)S(1)}, f32[256,2048]{1,0:T(8,128)S(1)}) custom-call(bf16[4,256,2048]{2,1,0:T(8,128)(2,1)S(1)} %bitcast.183, bf16[256,2048]{1,0:T(8,128)(2,1)S(1)} %bitcast.182, f32[1,2048]{1,0:T(1,128)S(1)} %reshape.412.refs_2_.refs_3_), custom_call_target="tpu_custom_call" | custom-call | tf_op jit(solution)/shard_map/fold_forward/pallas_call | solution.py:521
  264.5 2.1 copy-done.9
  266.6 17.3 %fusion.46 = f32[1024,2816]{1,0:T(8,128)S(1)} fusion(bf16[1024,2048]{1,0:T(8,128)(2,1)} %bitcast.185, bf16[2048,2816]{1,0:T(8,128)(2,1)} %all-gather.9.cloned.1.call-done), kind=kOutput, calls=%fused_computation.233 | convolution fusion | flops 11811160064 | bytes 27262976 | tf_op jit(solution)/shard_map/dot_general | solution.py:25
  284.0 1.8 multiply_convert_fusion.2
  285.8 3.5 copy-done.23
  290.9 8.1 %convolution_convert_fusion.1 = bf16[1408,2048]{1,0:T(8,128)(2,1)} fusion(bf16[1024,1408]{1,0:T(8,128)(2,1)S(1)} %multiply_convert_fusion.2, bf16[1024,2048]{1,0:T(8,128)(2,1)S(1)} %copy-done.43), kind=kOutput, calls=%fused_computation.9 | convolution fusion | flops 5908463616 | bytes 12845056 | tf_op jit(solution)/shard_map/dot_general | solution.py:33
  299.1 15.4 %multiply_convert_fusion.1 = (bf16[1024,1408]{1,0:T(8,128)(2,1)S(1)}, bf16[1024,1408]{1,0:T(8,128)(2,1)}) fusion(f32[1024,2816]{1,0:T(8,128)} %copy-done.23, bf16[1024,2048]{1,0:T(8,128)(2,1)} %copy-done.42, bf16[1408,2048]{1,0:T(8,128)(2,1)} %all-gather.11.cloned.1.call-done), kind=kOutput, calls=%fused_computation.12 | convolution fusion | flops 5924323328 | bytes 27262976 | tf_op jit(solution)/shard_map/dot_general | solution.py:29
  316.1 17.8 %convolution_convert_fusion.3 = bf16[1024,2048]{1,0:T(8,128)(2,1)} fusion(bf16[2048,2816]{1,0:T(8,128)(2,1)} %all-gather.9.cloned.1.call-done, bf16[1024,1408]{1,0:T(8,128)(2,1)} %get-tuple-element.121, bf16[1024,1408]{1,0:T(8,128)(2,1)S(1)} %get-tuple-element.120), kind=kOutput, calls=%fused_computation.19 | convolution fusion | flops 11824791552 | bytes 21495808 | tf_op jit(solution)/shard_map/dot_general | solution.py:29
  334.1 11.5 %convolution_convert_fusion.2 = bf16[1024,2816]{1,0:T(8,128)(2,1)} fusion(pred[]{:T(512)S(6)} %eq.86, bf16[1024,1408]{1,0:T(8,128)(2,1)} %get-tuple-element.121, bf16[1024,1408]{1,0:T(8,128)(2,1)} %copy-done.59, bf16[1024,256]{1,0:T(8,128)(2,1)S(1)} %get-tuple-element.138, bf16[1024,256]{1,0:T(8,128)(2,1)S(1)} %get-tuple-element.139, ...), kind=kOutput, calls=%fused_computation.16 | convolution fusion | flops 5937823744 | bytes 15728641 | tf_op jit(solution)/shard_map/dot_general | solution.py:33
  347.5 11.1 %convolution_convert_fusion.4 = bf16[1024,2048]{1,0:T(8,128)(2,1)} fusion(bf16[1024,1408]{1,0:T(8,128)(2,1)S(1)} %copy-done.27, bf16[1408,2048]{1,0:T(8,128)(2,1)} %all-gather.11.cloned.1.call-done), kind=kOutput, calls=%fused_computation.20 | convolution fusion | flops 5907677184 | bytes 12845056 | tf_op jit(solution)/shard_map/dot_general | solution.py:25
  358.6 8.6 %add_convert_fusion = bf16[1024,2816]{1,0:T(8,128)(2,1)} fusion(bf16[1024,2816]{1,0:T(8,128)(2,1)S(1)} %collective-permute-done.19, bf16[1024,1024]{1,0:T(8,128)(2,1)S(1)} %broadcast_select_fusion, bf16[1024,1408]{1,0:T(8,128)(2,1)S(1)} %copy-done.61, bf16[1024,1408]{1,0:T(8,128)(2,1)S(1)} %copy-done.60), kind=kOutput, calls=%fused_computation | convolution fusion | flops 5925765120 | bytes 19398656 | tf_op jit(solution)/shard_map/dot_general | solution.py:33
  369.1 2.2 copy-done.8
  371.3 76.8 %fold_backward.1 = (bf16[4,256,2048]{2,1,0:T(8,128)(2,1)S(1)}, f32[256,2048]{1,0:T(8,128)S(1)}, f32[1,2048]{1,0:T(1,128)S(1)}) custom-call(bf16[4,256,2048]{2,1,0:T(8,128)(2,1)S(1)} %bitcast.184, bf16[256,2048]{1,0:T(8,128)(2,1)} %bitcast.18.refs_1_, f32[256,2048]{1,0:T(8,128)S(1)} %copy-done.4, f32[1,2048]{1,0:T(1,128)S(1)} %reshape.412.refs_2_.refs_3_), custom_call_target="tpu_custom_call" | custom-call | tf_op jit(solution)/shard_map/fold_backward/pallas_call | solution.py:521
  450.4 5.7 multiply_reduce_fusion
  456.2 3.1 subtract_convert_fusion.grad_output
  459.3 2.4 collective-permute-done.20
  463.1 2.4 convolution_convert_fusion.6
  472.7 2.2 copy-done.1
  476.4 21.2 %mixer_backward.1 = (bf16[1024,1536]{1,0:T(8,128)(2,1)S(1)}, f32[64,1024]{1,0:T(8,128)S(1)}) custom-call(s32[1]{0:T(128)} %bitcast.mine, bf16[1024,2048]{1,0:T(8,128)(2,1)S(1)} %copy-done.1, bf16[1024,2048]{1,0:T(8,128)(2,1)S(1)} %copy-done.1, bf16[1024,2048]{1,0:T(8,128)(2,1)S(1)} %copy-done.1, bf16[1024,512]{1,0:T(8,128)(2,1)S(1)} %copy-done.11, ...), custom_call_target="tpu_custom_call" | custom-call | flops 2097152000 | bytes 10485760 | tf_op jit(solution)/shard_map/mixer_backward/pallas_call | solution.py:310
  499.3 11.5 %convolution_convert_fusion = bf16[2048,2048]{1,0:T(8,128)(2,1)} fusion(bf16[1024,2048]{1,0:T(8,128)(2,1)S(1)} %copy-done.20, bf16[1024,512]{1,0:T(8,128)(2,1)S(1)} %copy-done.32, bf16[1024,1536]{1,0:T(8,128)(2,1)S(1)} %get-tuple-element.75), kind=kOutput, calls=%fused_computation.8 | convolution fusion | flops 8602517504 | bytes 16777216 | tf_op jit(solution)/shard_map/dot_general | solution.py:33
  512.5 2.6 pad_maximum_fusion.1
  516.2 12.0 %fusion.47 = f32[1024,2048]{1,0:T(8,128)S(1)} fusion(bf16[1024,2048]{1,0:T(8,128)(2,1)S(1)} %pad_maximum_fusion.1, bf16[2048,2048]{1,0:T(8,128)(2,1)} %all-gather.7.cloned.1.call-done), kind=kOutput, calls=%fused_computation.234 | convolution fusion | flops 8589934592 | bytes 20971520 | tf_op jit(solution)/shard_map/dot_general | solution.py:29
  528.3 3.2 fusion.3
  532.0 2.9 fusion.48
  536.5 4.5 collective-permute-done.29
  541.4 3.7 collective-permute-done.30
  545.2 2.5 collective-permute-start.31
  547.8 3.0 collective-permute-done.31
  555.7 9.1 %collective-permute-done.25 = bf16[128,2048]{1,0:T(8,128)(2,1)S(1)} collective-permute-done((bf16[128,2048]{1,0:T(8,128)(2,1)S(1)}, bf16[128,2048]{1,0:T(8,128)(2,1)S(1)}, u32[]{:S(2)}, u32[]{:S(2)}) %collective-permute-start.25) | collective-permute-done | bytes 524320 | tf_op jit(solution)/shard_map/ppermute | solution.py:542
  573.4 15.9 %collective-permute-done.28 = bf16[256,2048]{1,0:T(8,128)(2,1)S(1)} collective-permute-done((bf16[256,2048]{1,0:T(8,128)(2,1)}, bf16[256,2048]{1,0:T(8,128)(2,1)S(1)}, u32[]{:S(2)}, u32[]{:S(2)}) %collective-permute-start.28) | collective-permute-done | bytes 1048608 | tf_op jit(solution)/shard_map/ppermute | solution.py:542
  589.3 1.8 collective-permute-done.26
  591.1 3.1 convert_add_fusion
  594.2 2.2 copy.74
  597.9 2.9 copy.76
  600.8 1.7 fusion.11
  606.3 4.9 fusion.17
  612.7 3.2 collective-permute-done.38
  625.4 1.9 collective-permute-done.36
  627.3 2.7 collective-permute-done.35
  631.2 2.4 reshape.416
  633.6 2.9 copy.117
  (369 shorter events, 112.1 us)
Async XLA Ops:
  7.2 108.7 %all-gather.5.cloned.1.call-start = ((), (), s32[]{:S(2)}) async-start(), calls=%async_computation.4 | async-start | bytes 2359296 | tf_op jit(solution)/shard_map/all_gather | solution.py:734
  7.9 117.9 %all-gather.7.cloned.1.call-start = ((), (), s32[]{:S(2)}) async-start(), calls=%async_computation.5 | async-start | bytes 9437184 | tf_op jit(solution)/shard_map/all_gather | solution.py:738
  15.4 11.1 %collective-permute-start.11 = (bf16[64,2048]{1,0:T(8,128)(2,1)S(1)}, bf16[64,2048]{1,0:T(8,128)(2,1)S(1)}, u32[]{:S(2)}, u32[]{:S(2)}) collective-permute-start(bf16[64,2048]{1,0:T(8,128)(2,1)S(1)} %bitcast.227), channel_id=1, source_target_pairs={{0,24},{8,16},{16,8},{24,0},{1,25},{9,17},{17,9},{25,1},{2,26},{10... | collective-permute-start | bytes 786440 | tf_op jit(solution)/shard_map/ppermute | solution.py:542
  19.5 11.8 %collective-permute-start.10 = (bf16[64,2048]{1,0:T(8,128)(2,1)S(1)}, bf16[64,2048]{1,0:T(8,128)(2,1)S(1)}, u32[]{:S(2)}, u32[]{:S(2)}) collective-permute-start(bf16[64,2048]{1,0:T(8,128)(2,1)S(1)} %bitcast.228), channel_id=1, source_target_pairs={{0,16},{8,24},{16,0},{24,8},{1,17},{9,25},{17,1},{25,9},{2,18},{10... | collective-permute-start | bytes 786440 | tf_op jit(solution)/shard_map/ppermute | solution.py:542
  20.2 11.3 %collective-permute-start.9 = (bf16[64,2048]{1,0:T(8,128)(2,1)S(1)}, bf16[64,2048]{1,0:T(8,128)(2,1)S(1)}, u32[]{:S(2)}, u32[]{:S(2)}) collective-permute-start(bf16[64,2048]{1,0:T(8,128)(2,1)S(1)} %bitcast.229), channel_id=1, source_target_pairs={{0,8},{8,0},{16,24},{24,16},{1,9},{9,1},{17,25},{25,17},{2,10},{10... | collective-permute-start | bytes 786440 | tf_op jit(solution)/shard_map/ppermute | solution.py:542
  33.0 233.6 %all-gather.9.cloned.1.call-start = ((), (), s32[]{:S(2)}) async-start(), calls=%async_computation.6 | async-start | bytes 12976128 | tf_op jit(solution)/shard_map/all_gather | solution.py:740
  37.2 12.3 %collective-permute-start.18 = (bf16[64,2816]{1,0:T(8,128)(2,1)S(1)}, bf16[64,2816]{1,0:T(8,128)(2,1)S(1)}, u32[]{:S(2)}, u32[]{:S(2)}) collective-permute-start(bf16[64,2816]{1,0:T(8,128)(2,1)S(1)} %bitcast.216), channel_id=1, source_target_pairs={{0,24},{8,16},{16,8},{24,0},{1,25},{9,17},{17,9},{25,1},{2,26},{10... | collective-permute-start | bytes 1081352 | tf_op jit(solution)/shard_map/ppermute | solution.py:542
  39.1 17.0 %collective-permute-start.17 = (bf16[64,2816]{1,0:T(8,128)(2,1)S(1)}, bf16[64,2816]{1,0:T(8,128)(2,1)S(1)}, u32[]{:S(2)}, u32[]{:S(2)}) collective-permute-start(bf16[64,2816]{1,0:T(8,128)(2,1)S(1)} %bitcast.217), channel_id=1, source_target_pairs={{0,16},{8,24},{16,0},{24,8},{1,17},{9,25},{17,1},{25,9},{2,18},{10... | collective-permute-start | bytes 1081352 | tf_op jit(solution)/shard_map/ppermute | solution.py:542
  40.4 16.0 %collective-permute-start.16 = (bf16[64,2816]{1,0:T(8,128)(2,1)S(1)}, bf16[64,2816]{1,0:T(8,128)(2,1)S(1)}, u32[]{:S(2)}, u32[]{:S(2)}) collective-permute-start(bf16[64,2816]{1,0:T(8,128)(2,1)S(1)} %bitcast.218), channel_id=1, source_target_pairs={{0,8},{8,0},{16,24},{24,16},{1,9},{9,1},{17,25},{25,17},{2,10},{10... | collective-permute-start | bytes 1081352 | tf_op jit(solution)/shard_map/ppermute | solution.py:542
  56.8 16.0 %copy-start.2 = (bf16[1,256,2048]{2,1,0:T(8,128)(2,1)S(1)}, bf16[1,256,2048]{2,1,0:T(8,128)(2,1)}, u32[]{:S(2)}) copy-start(bf16[1,256,2048]{2,1,0:T(8,128)(2,1)} %param.17) | copy-start | bytes 3145732
  58.1 241.0 %all-gather.11.cloned.1.call-start = ((), (), s32[]{:S(2)}) async-start(), calls=%async_computation.7 | async-start | bytes 6488064 | tf_op jit(solution)/shard_map/all_gather | solution.py:741
  58.9 1.2 collective-permute-start.4
  60.1 3.8 collective-permute-start.5
  64.0 7.1 %collective-permute-start.6 = (bf16[4,1608]{1,0:T(4,128)(2,1)S(1)}, bf16[4,1608]{1,0:T(4,128)(2,1)S(1)}, u32[]{:S(2)}, u32[]{:S(2)}) collective-permute-start(bf16[4,1608]{1,0:T(4,128)(2,1)S(1)} %pad_maximum_fusion.28), channel_id=1, source_target_pairs={{0,4},{1,5},{2,6},{3,7},{4,0},{5,1},{6,2},{7,3},{8,12},{9,13},{10,... | collective-permute-start | bytes 38600 | tf_op jit(solution)/shard_map/ppermute | solution.py:580
  71.2 6.8 %collective-permute-start.7 = (bf16[8,1608]{1,0:T(8,128)(2,1)S(1)}, bf16[8,1608]{1,0:T(8,128)(2,1)S(1)}, u32[]{:S(2)}, u32[]{:S(2)}) collective-permute-start(bf16[8,1608]{1,0:T(8,128)(2,1)S(1)} %pad_maximum_fusion.27), channel_id=1, source_target_pairs={{0,8},{8,0},{16,24},{24,16},{1,9},{9,1},{17,25},{25,17},{2,10},{10... | collective-permute-start | bytes 77192 | tf_op jit(solution)/shard_map/ppermute | solution.py:580
  75.9 28.9 %collective-permute-start = (bf16[256,2048]{1,0:T(8,128)(2,1)S(1)}, bf16[256,2048]{1,0:T(8,128)(2,1)}, u32[]{:S(2)}, u32[]{:S(2)}) collective-permute-start(bf16[256,2048]{1,0:T(8,128)(2,1)S(1)} %copy.67), channel_id=1, source_target_pairs={{0,8},{8,0},{16,24},{24,16},{1,9},{9,1},{17,25},{25,17},{2,10},{10... | collective-permute-start | bytes 3145736 | tf_op jit(solution)/shard_map/ppermute | solution.py:542
  76.5 23.7 %collective-permute-start.1 = (bf16[256,2048]{1,0:T(8,128)(2,1)S(1)}, bf16[256,2048]{1,0:T(8,128)(2,1)}, u32[]{:S(2)}, u32[]{:S(2)}) collective-permute-start(bf16[256,2048]{1,0:T(8,128)(2,1)S(1)} %copy.67), channel_id=1, source_target_pairs={{0,16},{8,24},{16,0},{24,8},{1,17},{9,25},{17,1},{25,9},{2,18},{10... | collective-permute-start | bytes 3145736 | tf_op jit(solution)/shard_map/ppermute | solution.py:542
  78.0 20.7 %collective-permute-start.8 = (bf16[16,1608]{1,0:T(8,128)(2,1)S(1)}, bf16[16,1608]{1,0:T(8,128)(2,1)S(1)}, u32[]{:S(2)}, u32[]{:S(2)}) collective-permute-start(bf16[16,1608]{1,0:T(8,128)(2,1)S(1)} %pad_maximum_fusion.26), channel_id=1, source_target_pairs={{0,16},{8,24},{16,0},{24,8},{1,17},{9,25},{17,1},{25,9},{2,18},{10... | collective-permute-start | bytes 154376 | tf_op jit(solution)/shard_map/ppermute | solution.py:580
  102.1 9.5 %collective-permute-start.2 = (bf16[128,2048]{1,0:T(8,128)(2,1)}, bf16[128,2048]{1,0:T(8,128)(2,1)}, u32[]{:S(2)}, u32[]{:S(2)}) collective-permute-start(bf16[128,2048]{1,0:T(8,128)(2,1)} %slice.208), channel_id=1, source_target_pairs={{0,8},{8,0},{16,24},{24,16},{1,9},{9,1},{17,25},{25,17},{2,10},{10... | collective-permute-start | bytes 1572872 | tf_op jit(solution)/shard_map/ppermute | solution.py:542
  104.4 16.0 %copy-start.37 = (bf16[16,2048]{1,0:T(8,128)(2,1)}, bf16[16,2048]{1,0:T(8,128)(2,1)S(1)}, u32[]{:S(2)}) copy-start(bf16[16,2048]{1,0:T(8,128)(2,1)S(1)} %reshape.381) | copy-start | bytes 196612
  104.5 19.1 %copy-start.47 = (bf16[256,16]{1,0:T(8,128)(2,1)}, bf16[256,16]{1,0:T(8,128)(2,1)S(1)}, u32[]{:S(2)}) copy-start(bf16[256,16]{1,0:T(8,128)(2,1)S(1)} %reshape.378) | copy-start | bytes 24580
  104.7 262.6 %reduce-scatter.5.cloned.1.call-start = ((), (), s32[]{:S(2)}) async-start(), calls=%async_computation.8 | async-start | bytes 6488064 | tf_op jit(solution)/shard_map/reduce_scatter | solution.py:833
  105.8 9.2 %collective-permute-start.3 = (bf16[128,2048]{1,0:T(8,128)(2,1)S(1)}, bf16[128,2048]{1,0:T(8,128)(2,1)S(1)}, u32[]{:S(2)}, u32[]{:S(2)}) collective-permute-start(bf16[128,2048]{1,0:T(8,128)(2,1)S(1)} %slice.209), channel_id=1, source_target_pairs={{0,16},{8,24},{16,0},{24,8},{1,17},{9,25},{17,1},{25,9},{2,18},{10... | collective-permute-start | bytes 1572872 | tf_op jit(solution)/shard_map/ppermute | solution.py:542
  123.6 17.6 %copy-start.45 = (bf16[1024,16]{0,1:T(8,128)(2,1)}, bf16[1024,16]{0,1:T(8,128)(2,1)S(1)}, u32[]{:S(2)}) copy-start(bf16[1024,16]{0,1:T(8,128)(2,1)S(1)} %convolution_convert_fusion.8) | copy-start | bytes 98308
  125.8 15.5 %copy-start.6 = (f32[128,1024]{1,0:T(8,128)S(1)}, f32[128,1024]{1,0:T(8,128)}, u32[]{:S(2)}) copy-start(f32[128,1024]{1,0:T(8,128)} %pad_maximum_fusion.22.rate) | copy-start | bytes 1572868
  125.8 34.4 %collective-permute-start.12 = (bf16[256,2048]{1,0:T(8,128)(2,1)}, bf16[256,2048]{1,0:T(8,128)(2,1)S(1)}, u32[]{:S(2)}, u32[]{:S(2)}) collective-permute-start(bf16[256,2048]{1,0:T(8,128)(2,1)} %bitcast.18.refs_1_), channel_id=1, source_target_pairs={{0,8},{8,0},{16,24},{24,16},{1,9},{9,1},{17,25},{25,17},{2,10},{10... | collective-permute-start | bytes 3145736 | tf_op jit(solution)/shard_map/ppermute | solution.py:542
  127.3 30.8 %collective-permute-start.13 = (bf16[256,2048]{1,0:T(8,128)(2,1)}, bf16[256,2048]{1,0:T(8,128)(2,1)S(1)}, u32[]{:S(2)}, u32[]{:S(2)}) collective-permute-start(bf16[256,2048]{1,0:T(8,128)(2,1)} %bitcast.18.refs_1_), channel_id=1, source_target_pairs={{0,16},{8,24},{16,0},{24,8},{1,17},{9,25},{17,1},{25,9},{2,18},{10... | collective-permute-start | bytes 3145736 | tf_op jit(solution)/shard_map/ppermute | solution.py:542
  141.2 12.0 %copy-start = (bf16[1024,2048]{1,0:T(8,128)(2,1)}, bf16[1024,2048]{1,0:T(8,128)(2,1)S(1)}, u32[]{:S(2)}) copy-start(bf16[1024,2048]{1,0:T(8,128)(2,1)S(1)} %get-tuple-element.219.query.key.value) | copy-start | bytes 12582916
  141.2 12.2 %copy-start.28 = (f32[1024,2048]{1,0:T(8,128)}, f32[1024,2048]{1,0:T(8,128)S(1)}, u32[]{:S(2)}) copy-start(f32[1024,2048]{1,0:T(8,128)S(1)} %get-tuple-element.220) | copy-start | bytes 25165828
  158.1 13.6 %collective-permute-start.14 = (bf16[128,2048]{1,0:T(8,128)(2,1)S(1)}, bf16[128,2048]{1,0:T(8,128)(2,1)S(1)}, u32[]{:S(2)}, u32[]{:S(2)}) collective-permute-start(bf16[128,2048]{1,0:T(8,128)(2,1)S(1)} %slice.212), channel_id=1, source_target_pairs={{0,8},{8,0},{16,24},{24,16},{1,9},{9,1},{17,25},{25,17},{2,10},{10... | collective-permute-start | bytes 1572872 | tf_op jit(solution)/shard_map/ppermute | solution.py:542
  160.2 13.3 %collective-permute-start.15 = (bf16[128,2048]{1,0:T(8,128)(2,1)S(1)}, bf16[128,2048]{1,0:T(8,128)(2,1)S(1)}, u32[]{:S(2)}, u32[]{:S(2)}) collective-permute-start(bf16[128,2048]{1,0:T(8,128)(2,1)S(1)} %slice.213), channel_id=1, source_target_pairs={{0,16},{8,24},{16,0},{24,8},{1,17},{9,25},{17,1},{25,9},{2,18},{10... | collective-permute-start | bytes 1572872 | tf_op jit(solution)/shard_map/ppermute | solution.py:542
  299.0 173.3 %reduce-scatter.7.cloned.1.call-start = ((), (), s32[]{:S(2)}) async-start(), calls=%async_computation.9 | async-start | bytes 7208960 | tf_op jit(solution)/shard_map/reduce_scatter | solution.py:633
  316.1 17.8 %copy-start.10 = (bf16[4,256,2048]{2,1,0:T(8,128)(2,1)S(1)}, bf16[4,256,2048]{2,1,0:T(8,128)(2,1)}, u32[]{:S(2)}) copy-start(bf16[4,256,2048]{2,1,0:T(8,128)(2,1)} %copy-done.9) | copy-start | bytes 12582916
  345.7 12.9 %collective-permute-start.19 = (bf16[1024,2816]{1,0:T(8,128)(2,1)}, bf16[1024,2816]{1,0:T(8,128)(2,1)S(1)}, u32[]{:S(2)}, u32[]{:S(2)}) collective-permute-start(bf16[1024,2816]{1,0:T(8,128)(2,1)} %convolution_convert_fusion.2), channel_id=1, source_target_pairs={{0,1},{1,0},{2,3},{3,2},{4,5},{5,4},{6,7},{7,6},{8,9},{9,8},{10,11... | collective-permute-start | bytes 17301512 | tf_op jit(solution)/shard_map/ppermute | solution.py:580
  347.5 11.1 %copy-start.61 = (bf16[1024,1408]{1,0:T(8,128)(2,1)S(1)}, bf16[1024,1408]{1,0:T(8,128)(2,1)}, u32[]{:S(2)}) copy-start(bf16[1024,1408]{1,0:T(8,128)(2,1)} %get-tuple-element.121) | copy-start | bytes 8650756
  367.3 143.6 %reduce-scatter.9.cloned.1.call-start = ((), (), s32[]{:S(2)}) async-start(), calls=%async_computation.10 | async-start | bytes 1310720 | tf_op jit(solution)/shard_map/reduce_scatter | solution.py:633
  371.3 76.8 %copy-start.25 = (bf16[1024,2048]{1,0:T(8,128)(2,1)S(1)}, bf16[1024,2048]{1,0:T(8,128)(2,1)}, u32[]{:S(2)}) copy-start(bf16[1024,2048]{1,0:T(8,128)(2,1)} %convolution_convert_fusion.4) | copy-start | bytes 12582916
  448.3 13.4 %collective-permute-start.20 = (bf16[128,2048]{1,0:T(8,128)(2,1)S(1)}, bf16[128,2048]{1,0:T(8,128)(2,1)S(1)}, u32[]{:S(2)}, u32[]{:S(2)}) collective-permute-start(bf16[128,2048]{1,0:T(8,128)(2,1)S(1)} %get-tuple-element.135), channel_id=1, source_target_pairs={{0,8},{8,0},{16,24},{24,16},{1,9},{9,1},{17,25},{25,17},{2,10},{10... | collective-permute-start | bytes 1572872 | tf_op jit(solution)/shard_map/ppermute | solution.py:542
  449.9 13.3 %collective-permute-start.21 = (bf16[128,2048]{1,0:T(8,128)(2,1)S(1)}, bf16[128,2048]{1,0:T(8,128)(2,1)S(1)}, u32[]{:S(2)}, u32[]{:S(2)}) collective-permute-start(bf16[128,2048]{1,0:T(8,128)(2,1)S(1)} %get-tuple-element.134), channel_id=1, source_target_pairs={{0,16},{8,24},{16,0},{24,8},{1,17},{9,25},{17,1},{25,9},{2,18},{10... | collective-permute-start | bytes 1572872 | tf_op jit(solution)/shard_map/ppermute | solution.py:542
  466.1 4.7 collective-permute-start.24
  467.7 30.0 %collective-permute-start.22 = (bf16[256,2048]{1,0:T(8,128)(2,1)}, bf16[256,2048]{1,0:T(8,128)(2,1)}, u32[]{:S(2)}, u32[]{:S(2)}) collective-permute-start(bf16[256,2048]{1,0:T(8,128)(2,1)} %pad_maximum_fusion.15), channel_id=1, source_target_pairs={{0,8},{8,0},{16,24},{24,16},{1,9},{9,1},{17,25},{25,17},{2,10},{10... | collective-permute-start | bytes 3145736 | tf_op jit(solution)/shard_map/ppermute | solution.py:542
  469.1 28.6 %collective-permute-start.23 = (bf16[256,2048]{1,0:T(8,128)(2,1)}, bf16[256,2048]{1,0:T(8,128)(2,1)}, u32[]{:S(2)}, u32[]{:S(2)}) collective-permute-start(bf16[256,2048]{1,0:T(8,128)(2,1)} %pad_maximum_fusion.16), channel_id=1, source_target_pairs={{0,16},{8,24},{16,0},{24,8},{1,17},{9,25},{17,1},{25,9},{2,18},{10... | collective-permute-start | bytes 3145736 | tf_op jit(solution)/shard_map/ppermute | solution.py:542
  472.4 144.7 %reduce-scatter.11.cloned.1.call-start = ((), (), s32[]{:S(2)}) async-start(), calls=%async_computation.11 | async-start | bytes 9437184 | tf_op jit(solution)/shard_map/reduce_scatter | solution.py:889
  476.4 22.9 %copy-start.20 = (bf16[1024,2048]{1,0:T(8,128)(2,1)S(1)}, bf16[1024,2048]{1,0:T(8,128)(2,1)}, u32[]{:S(2)}) copy-start(bf16[1024,2048]{1,0:T(8,128)(2,1)} %copy-done.19) | copy-start | bytes 12582916
  476.4 22.9 %copy-start.32 = (bf16[1024,512]{1,0:T(8,128)(2,1)S(1)}, bf16[1024,512]{1,0:T(8,128)(2,1)}, u32[]{:S(2)}) copy-start(bf16[1024,512]{1,0:T(8,128)(2,1)} %get-tuple-element.122) | copy-start | bytes 3145732
  516.2 12.0 %copy-start.22 = (bf16[1024,2048]{1,0:T(8,128)(2,1)S(1)}, bf16[1024,2048]{1,0:T(8,128)(2,1)}, u32[]{:S(2)}) copy-start(bf16[1024,2048]{1,0:T(8,128)(2,1)} %constant_dynamic-update-slice_fusion) | copy-start | bytes 12582916
  516.2 12.1 %copy-start.38 = (bf16[16,2048]{1,0:T(8,128)(2,1)S(1)}, bf16[16,2048]{1,0:T(8,128)(2,1)}, u32[]{:S(2)}) copy-start(bf16[16,2048]{1,0:T(8,128)(2,1)} %copy-done.37) | copy-start | bytes 196612
  516.2 12.1 %copy-start.49 = (f32[1024]{0:T(1024)S(1)}, f32[1024]{0:T(1024)}, u32[]{:S(2)}) copy-start(f32[1024]{0:T(1024)} %copy-done.48) | copy-start | bytes 12292
  535.1 12.6 %copy-start.40 = (f32[32,64]{1,0:T(8,128)S(1)}, f32[32,64]{1,0:T(8,128)}, u32[]{:S(2)}) copy-start(f32[32,64]{1,0:T(8,128)} %copy-done.39) | copy-start | bytes 24580
  536.4 4.6 collective-permute-start.29
  541.1 4.1 collective-permute-start.30
  545.2 5.7 collective-permute-start.31
  550.9 4.7 collective-permute-start.32
  554.0 10.8 %collective-permute-start.25 = (bf16[128,2048]{1,0:T(8,128)(2,1)S(1)}, bf16[128,2048]{1,0:T(8,128)(2,1)S(1)}, u32[]{:S(2)}, u32[]{:S(2)}) collective-permute-start(bf16[128,2048]{1,0:T(8,128)(2,1)S(1)} %get-tuple-element.128), channel_id=1, source_target_pairs={{0,16},{8,24},{16,0},{24,8},{1,17},{9,25},{17,1},{25,9},{2,18},{10... | collective-permute-start | bytes 1572872 | tf_op jit(solution)/shard_map/ppermute | solution.py:542
  554.2 10.9 %collective-permute-start.27 = (bf16[128,2048]{1,0:T(8,128)(2,1)S(1)}, bf16[128,2048]{1,0:T(8,128)(2,1)S(1)}, u32[]{:S(2)}, u32[]{:S(2)}) collective-permute-start(bf16[128,2048]{1,0:T(8,128)(2,1)S(1)} %get-tuple-element.127), channel_id=1, source_target_pairs={{0,8},{8,0},{16,24},{24,16},{1,9},{9,1},{17,25},{25,17},{2,10},{10... | collective-permute-start | bytes 1572872 | tf_op jit(solution)/shard_map/ppermute | solution.py:542
  555.6 15.0 %collective-permute-start.33 = (f32[1,1352]{1,0:T(1,128)S(1)}, f32[1,1352]{1,0:T(1,128)S(1)}, u32[]{:S(2)}, u32[]{:S(2)}) collective-permute-start(f32[1,1352]{1,0:T(1,128)S(1)} %broadcast_select_fusion.13), channel_id=1, source_target_pairs={{0,1},{1,0},{2,3},{3,2},{4,5},{5,4},{6,7},{7,6},{8,9},{9,8},{10,11... | collective-permute-start | bytes 16232 | tf_op jit(solution)/shard_map/ppermute | solution.py:580
  567.8 21.5 %collective-permute-start.28 = (bf16[256,2048]{1,0:T(8,128)(2,1)}, bf16[256,2048]{1,0:T(8,128)(2,1)S(1)}, u32[]{:S(2)}, u32[]{:S(2)}) collective-permute-start(bf16[256,2048]{1,0:T(8,128)(2,1)} %pad_maximum_fusion.20), channel_id=1, source_target_pairs={{0,16},{8,24},{16,0},{24,8},{1,17},{9,25},{17,1},{25,9},{2,18},{10... | collective-permute-start | bytes 3145736 | tf_op jit(solution)/shard_map/ppermute | solution.py:542
  570.3 20.8 %collective-permute-start.26 = (bf16[256,2048]{1,0:T(8,128)(2,1)}, bf16[256,2048]{1,0:T(8,128)(2,1)S(1)}, u32[]{:S(2)}, u32[]{:S(2)}) collective-permute-start(bf16[256,2048]{1,0:T(8,128)(2,1)} %pad_maximum_fusion.19), channel_id=1, source_target_pairs={{0,8},{8,0},{16,24},{24,16},{1,9},{9,1},{17,25},{25,17},{2,10},{10... | collective-permute-start | bytes 3145736 | tf_op jit(solution)/shard_map/ppermute | solution.py:542
  602.7 10.0 %collective-permute-start.39 = (bf16[64,2816]{1,0:T(8,128)(2,1)S(1)}, bf16[64,2816]{1,0:T(8,128)(2,1)S(1)}, u32[]{:S(2)}, u32[]{:S(2)}) collective-permute-start(bf16[64,2816]{1,0:T(8,128)(2,1)S(1)} %get-tuple-element.164), channel_id=1, source_target_pairs={{0,24},{8,16},{16,8},{24,0},{1,25},{9,17},{17,9},{25,1},{2,26},{10... | collective-permute-start | bytes 1081352 | tf_op jit(solution)/shard_map/ppermute | solution.py:542
  603.5 12.5 %collective-permute-start.38 = (bf16[64,2816]{1,0:T(8,128)(2,1)S(1)}, bf16[64,2816]{1,0:T(8,128)(2,1)S(1)}, u32[]{:S(2)}, u32[]{:S(2)}) collective-permute-start(bf16[64,2816]{1,0:T(8,128)(2,1)S(1)} %get-tuple-element.165), channel_id=1, source_target_pairs={{0,16},{8,24},{16,0},{24,8},{1,17},{9,25},{17,1},{25,9},{2,18},{10... | collective-permute-start | bytes 1081352 | tf_op jit(solution)/shard_map/ppermute | solution.py:542
  604.8 11.7 %collective-permute-start.37 = (bf16[64,2816]{1,0:T(8,128)(2,1)S(1)}, bf16[64,2816]{1,0:T(8,128)(2,1)S(1)}, u32[]{:S(2)}, u32[]{:S(2)}) collective-permute-start(bf16[64,2816]{1,0:T(8,128)(2,1)S(1)} %get-tuple-element.166), channel_id=1, source_target_pairs={{0,8},{8,0},{16,24},{24,16},{1,9},{9,1},{17,25},{25,17},{2,10},{10... | collective-permute-start | bytes 1081352 | tf_op jit(solution)/shard_map/ppermute | solution.py:542
  618.3 9.0 %collective-permute-start.36 = (bf16[64,2048]{1,0:T(8,128)(2,1)S(1)}, bf16[64,2048]{1,0:T(8,128)(2,1)S(1)}, u32[]{:S(2)}, u32[]{:S(2)}) collective-permute-start(bf16[64,2048]{1,0:T(8,128)(2,1)S(1)} %get-tuple-element.180), channel_id=1, source_target_pairs={{0,24},{8,16},{16,8},{24,0},{1,25},{9,17},{17,9},{25,1},{2,26},{10... | collective-permute-start | bytes 786440 | tf_op jit(solution)/shard_map/ppermute | solution.py:542
  619.4 10.6 %collective-permute-start.35 = (bf16[64,2048]{1,0:T(8,128)(2,1)S(1)}, bf16[64,2048]{1,0:T(8,128)(2,1)S(1)}, u32[]{:S(2)}, u32[]{:S(2)}) collective-permute-start(bf16[64,2048]{1,0:T(8,128)(2,1)S(1)} %get-tuple-element.181), channel_id=1, source_target_pairs={{0,16},{8,24},{16,0},{24,8},{1,17},{9,25},{17,1},{25,9},{2,18},{10... | collective-permute-start | bytes 786440 | tf_op jit(solution)/shard_map/ppermute | solution.py:542
  620.8 10.0 %collective-permute-start.34 = (bf16[64,2048]{1,0:T(8,128)(2,1)S(1)}, bf16[64,2048]{1,0:T(8,128)(2,1)S(1)}, u32[]{:S(2)}, u32[]{:S(2)}) collective-permute-start(bf16[64,2048]{1,0:T(8,128)(2,1)S(1)} %get-tuple-element.182), channel_id=1, source_target_pairs={{0,8},{8,0},{16,24},{24,16},{1,9},{9,1},{17,25},{25,17},{2,10},{10... | collective-permute-start | bytes 786440 | tf_op jit(solution)/shard_map/ppermute | solution.py:542
  (46 other events, 140.1 us)
Sparse Core Ops, SparseCore 0:
  9.6 31.7 all-gather.4
  43.6 82.1 all-gather.6
  128.0 106.4 all-gather.8
  236.0 58.7 all-gather.10
  299.1 64.9 reduce-scatter.4
  367.4 102.3 reduce-scatter.6
  472.5 27.1 reduce-scatter.8
  511.0 90.3 reduce-scatter.10

commit v12 on v11

--- a/solution.py
+++ b/solution.py
@@ -893,7 +893,10 @@
     grad_normed = dot_nt(after(grad_pre, term_pre), w_mixer) + dot_nn(grad_reduced, w_squeeze)
     term_mixer = restored(jnp.sum(grad_normed * plain_one, axis=0))
     term_squeeze = restored(dot_tn(grad_reduced, normed))
-    grad_normed = restored(scattered(grad_normed.astype(BF16), ring))
+    grad_normed, _, (term_mixer, term_squeeze) = scattered(
+        grad_normed.astype(BF16), ring, term_bias, (term_mixer, term_squeeze)
+    )
+    grad_normed = restored(grad_normed)
     inputs_own = input_own.astype(F32)
     scale_own = rms_scale(inputs_own)
     scaled_one = grad_normed * restored(gain_one)
@@ -903,11 +906,18 @@
         - inputs_own * scale_own**3 * jnp.mean(scaled_one * inputs_own, axis=-1, keepdims=True)
     ).astype(BF16)
     pre_share = exchanged(pre_sum.reshape(ring, own, 4 * part), mine, ring)
-    pre_share = pre_share.reshape(ring, own, 4, part).transpose(2, 1, 0, 3)
-    query_share, key_share, value_share, swish_share = pre_share.reshape(4, own, width).astype(F32)
+
+    def joined_columns(blocks, first, size):
+        return jnp.concatenate(
+            [blocks[at, :, first : first + size] for at in range(ring)], axis=1
+        ).astype(F32)
+
+    query_share, key_share, value_share, swish_share = (
+        joined_columns(pre_share, at * part, part) for at in range(4)
+    )
     feed_share = exchanged(after(feed_sum, term_pre).reshape(ring, own, 2 * hidden_part), mine, ring)
-    gate_share = feed_share[:, :, :hidden_part].transpose(1, 0, 2).reshape(own, -1).astype(F32)
-    up_share = feed_share[:, :, hidden_part:].transpose(1, 0, 2).reshape(own, -1).astype(F32)
+    gate_share = joined_columns(feed_share, 0, hidden_part)
+    up_share = joined_columns(feed_share, hidden_part, hidden_part)
 
     def placed(array, size):
         full = jnp.zeros((HEADS, size) + array.shape[1:], F32)

time: 657 us -> 656 us (level)
  local copies, waits for them, and re-layouts: 85.4 us -> 72.4 us
  waiting for transfers between devices: 121 us -> 133 us
    ppermute x28, waiting for transfers between devices: 81.2 us -> 97.5 us  [swapped(): return lax.ppermute(block, 'seq', [(i, i ^ by) for i in range(ring)])]
    convert_element_type x4 -> x0, local copies, waits for them, and re-layouts: 7.81 us -> none  [the longest x2 5.36 us: local(): pre_share.reshape(4, own, width).astype(F32)]
    unnamed x154 -> x148, local copies, waits for them, and re-layouts: 42.4 us -> 37.9 us
  transfers between devices with their start and end apart: 48 -> 48, of which waited for: 30 -> 27; matrix products, arithmetic and copies ran while one was open for 36% -> 36% of each run, Pallas kernels for 30% -> 30%
where the time goes in v12:
time: 656 us; the launch traced here: 648 us
  Pallas kernels  196 us (30%)
  matrix products  145 us (22%)
  waiting for transfers between devices  133 us (20%)
  local copies, waits for them, and re-layouts  72.4 us (11%)
  starting transfers between devices  43.1 us (7%)
  other arithmetic  42.8 us (7%)
  between operations  16 us (2%)
    pallas_call x2, Pallas kernels, fold(): pl.pallas_call(functools.partial(fold_kernel, finish, len(given)), out_sh...  162 us
    ppermute x28, waiting for transfers between devices, swapped(): return lax.ppermute(block, 'seq', [(i, i ^ by) for i in range(ring)])  97.5 us
    dot_general x6, matrix products, dot_nt(): lax.dot_general(left, right, (((1,), (1,)), ((), ())), preferred_element_...  53.3 us
    dot_general x7, matrix products, dot_tn(): lax.dot_general(left, right, (((0,), (0,)), ((), ())), preferred_element_...  46 us
    dot_general x6, matrix products, dot_nn(): lax.dot_general(left, right, (((1,), (0,)), ((), ())), preferred_element_...  45.5 us
    unnamed x148, local copies, waits for them, and re-layouts  37.9 us
    ppermute x12, waiting for transfers between devices, flipped(): lax.ppermute(block, axis, [(i, i ^ by) for i in range(lax.axis_size(axis))])  32.9 us
    ppermute x28, starting transfers between devices, swapped(): return lax.ppermute(block, 'seq', [(i, i ^ by) for i in range(ring)])  31.1 us
  transfers between devices with their start and end apart: 48, of which 27 were waited for; matrix products, arithmetic and copies ran while one was open for 36% of the time, Pallas kernels for 30%

profile of v12, /device:TPU:0, one launch (start us, length us, event | category | flops | bytes accessed | tf_op | source)
XLA Modules:
  0.0 648.0 jit_solution(12370418698472642760)
XLA Ops:
  13.1 2.2 constant_dynamic-slice_fusion.18
  15.4 4.0 collective-permute-start.11
  20.5 6.0 collective-permute-done.11
  26.5 4.7 collective-permute-done.10
  34.2 3.0 constant_dynamic-slice_fusion.9
  37.2 1.8 collective-permute-start.18
  41.0 8.5 %collective-permute-done.18 = bf16[64,2816]{1,0:T(8,128)(2,1)S(1)} collective-permute-done((bf16[64,2816]{1,0:T(8,128)(2,1)S(1)}, bf16[64,2816]{1,0:T(8,128)(2,1)S(1)}, u32[]{:S(2)}, u32[]{:S(2)}) %collective-permute-start.18) | collective-permute-done | bytes 360480 | tf_op jit(solution)/shard_map/ppermute | solution.py:542
  49.5 6.6 %collective-permute-done.17 = bf16[64,2816]{1,0:T(8,128)(2,1)S(1)} collective-permute-done((bf16[64,2816]{1,0:T(8,128)(2,1)S(1)}, bf16[64,2816]{1,0:T(8,128)(2,1)S(1)}, u32[]{:S(2)}, u32[]{:S(2)}) %collective-permute-start.17) | collective-permute-done | bytes 360480 | tf_op jit(solution)/shard_map/ppermute | solution.py:542
  61.7 2.2 collective-permute-done.5
  64.0 2.5 collective-permute-start.6
  66.5 4.6 collective-permute-done.6
  79.7 19.1 %collective-permute-done.8 = bf16[16,1608]{1,0:T(8,128)(2,1)S(1)} collective-permute-done((bf16[16,1608]{1,0:T(8,128)(2,1)S(1)}, bf16[16,1608]{1,0:T(8,128)(2,1)S(1)}, u32[]{:S(2)}, u32[]{:S(2)}) %collective-permute-start.8) | collective-permute-done | bytes 51488 | tf_op jit(solution)/shard_map/ppermute | solution.py:580
  100.2 1.9 slice.292
  106.5 2.3 constant_dynamic-update-slice_fusion.3
  108.8 2.4 constant_dynamic-update-slice_fusion.2
  111.6 1.9 constant_dynamic-update-slice_fusion.1
  115.9 3.2 fusion.4
  123.5 2.3 all-gather.7.cloned.1.call-done
  128.7 12.5 %fusion.44 = (bf16[1024,2048]{1,0:T(8,128)(2,1)S(1)}, f32[1024,2048]{1,0:T(8,128)S(1)}) fusion(bf16[1024,2048]{1,0:T(8,128)(2,1)} %copy-done.18, bf16[2048,2048]{1,0:T(8,128)(2,1)} %all-gather.7.cloned.1.call-done), kind=kOutput, calls=%fused_computation.247 | convolution fusion | flops 8592031744 | bytes 25165824 | tf_op jit(solution)/shard_map/dot_general | solution.py:25
  141.2 11.9 %mixer_forward.1 = (f32[1024,512]{1,0:T(8,128)S(1)}, f32[128,1024]{1,0:T(8,128)S(1)}, f32[8,128,512]{2,1,0:T(8,128)S(1)}) custom-call(s32[1]{0:T(128)} %bitcast.mine, bf16[1024,2048]{1,0:T(8,128)(2,1)S(1)} %get-tuple-element.241.query.key.value, bf16[1024,2048]{1,0:T(8,128)(2,1)S(1)} %get-tuple-element.241.query.key.value, ...), custom_call_target="tpu_custom_call" | custom-call | flops 1048576000 | bytes 6291456 | tf_op jit(solution)/shard_map/mixer_forward/pallas_call | solution.py:285
  155.7 2.3 convolution_convert_fusion.5
  161.1 10.7 %collective-permute-done.14 = bf16[128,2048]{1,0:T(8,128)(2,1)S(1)} collective-permute-done((bf16[128,2048]{1,0:T(8,128)(2,1)S(1)}, bf16[128,2048]{1,0:T(8,128)(2,1)S(1)}, u32[]{:S(2)}, u32[]{:S(2)}) %collective-permute-start.14) | collective-permute-done | bytes 524320 | tf_op jit(solution)/shard_map/ppermute | solution.py:542
  171.8 1.7 collective-permute-done.15
  173.6 2.0 copy-done.41
  175.6 85.6 %fold_forward.1 = (bf16[4,256,2048]{2,1,0:T(8,128)(2,1)S(1)}, f32[256,2048]{1,0:T(8,128)S(1)}) custom-call(bf16[4,256,2048]{2,1,0:T(8,128)(2,1)S(1)} %bitcast.205, bf16[256,2048]{1,0:T(8,128)(2,1)S(1)} %bitcast.204, f32[1,2048]{1,0:T(1,128)S(1)} %reshape.401.refs_2_.refs_3_), custom_call_target="tpu_custom_call" | custom-call | tf_op jit(solution)/shard_map/fold_forward/pallas_call | solution.py:521
  262.6 2.1 copy-done.9
  264.6 17.3 %fusion.45 = f32[1024,2816]{1,0:T(8,128)S(1)} fusion(bf16[1024,2048]{1,0:T(8,128)(2,1)} %bitcast.207, bf16[2048,2816]{1,0:T(8,128)(2,1)} %all-gather.9.cloned.1.call-done), kind=kOutput, calls=%fused_computation.248 | convolution fusion | flops 11811160064 | bytes 27262976 | tf_op jit(solution)/shard_map/dot_general | solution.py:25
  282.0 1.8 multiply_convert_fusion.2
  283.8 3.5 copy-done.23
  288.9 8.1 %convolution_convert_fusion.1 = bf16[1408,2048]{1,0:T(8,128)(2,1)} fusion(bf16[1024,1408]{1,0:T(8,128)(2,1)S(1)} %multiply_convert_fusion.2, bf16[1024,2048]{1,0:T(8,128)(2,1)S(1)} %copy-done.42), kind=kOutput, calls=%fused_computation.9 | convolution fusion | flops 5908463616 | bytes 12845056 | tf_op jit(solution)/shard_map/dot_general | solution.py:33
  297.1 15.4 %multiply_convert_fusion.1 = (bf16[1024,1408]{1,0:T(8,128)(2,1)S(1)}, bf16[1024,1408]{1,0:T(8,128)(2,1)}) fusion(f32[1024,2816]{1,0:T(8,128)} %copy-done.23, bf16[1024,2048]{1,0:T(8,128)(2,1)} %copy-done.41, bf16[1408,2048]{1,0:T(8,128)(2,1)} %all-gather.11.cloned.1.call-done), kind=kOutput, calls=%fused_computation.12 | convolution fusion | flops 5924323328 | bytes 27262976 | tf_op jit(solution)/shard_map/dot_general | solution.py:29
  314.1 17.8 %convolution_convert_fusion.3 = bf16[1024,2048]{1,0:T(8,128)(2,1)} fusion(bf16[2048,2816]{1,0:T(8,128)(2,1)} %all-gather.9.cloned.1.call-done, bf16[1024,1408]{1,0:T(8,128)(2,1)} %get-tuple-element.133, bf16[1024,1408]{1,0:T(8,128)(2,1)S(1)} %get-tuple-element.132), kind=kOutput, calls=%fused_computation.19 | convolution fusion | flops 11824791552 | bytes 21495808 | tf_op jit(solution)/shard_map/dot_general | solution.py:29
  332.2 11.5 %convolution_convert_fusion.2 = bf16[1024,2816]{1,0:T(8,128)(2,1)} fusion(pred[]{:T(512)S(6)} %eq.86, bf16[1024,1408]{1,0:T(8,128)(2,1)} %get-tuple-element.133, bf16[1024,1408]{1,0:T(8,128)(2,1)} %copy-done.58, bf16[1024,256]{1,0:T(8,128)(2,1)S(1)} %get-tuple-element.150, bf16[1024,256]{1,0:T(8,128)(2,1)S(1)} %get-tuple-element.151, ...), kind=kOutput, calls=%fused_computation.16 | convolution fusion | flops 5937823744 | bytes 15728641 | tf_op jit(solution)/shard_map/dot_general | solution.py:33
  345.6 11.1 %convolution_convert_fusion.4 = bf16[1024,2048]{1,0:T(8,128)(2,1)} fusion(bf16[1024,1408]{1,0:T(8,128)(2,1)S(1)} %copy-done.27, bf16[1408,2048]{1,0:T(8,128)(2,1)} %all-gather.11.cloned.1.call-done), kind=kOutput, calls=%fused_computation.20 | convolution fusion | flops 5907677184 | bytes 12845056 | tf_op jit(solution)/shard_map/dot_general | solution.py:25
  356.6 8.6 %add_convert_fusion = bf16[1024,2816]{1,0:T(8,128)(2,1)} fusion(bf16[1024,2816]{1,0:T(8,128)(2,1)S(1)} %collective-permute-done.19, bf16[1024,1024]{1,0:T(8,128)(2,1)S(1)} %broadcast_select_fusion, bf16[1024,1408]{1,0:T(8,128)(2,1)S(1)} %copy-done.60, bf16[1024,1408]{1,0:T(8,128)(2,1)S(1)} %copy-done.59), kind=kOutput, calls=%fused_computation | convolution fusion | flops 5925765120 | bytes 19398656 | tf_op jit(solution)/shard_map/dot_general | solution.py:33
  367.1 2.2 copy-done.8
  369.3 76.7 %fold_backward.1 = (bf16[4,256,2048]{2,1,0:T(8,128)(2,1)S(1)}, f32[256,2048]{1,0:T(8,128)S(1)}, f32[1,2048]{1,0:T(1,128)S(1)}) custom-call(bf16[4,256,2048]{2,1,0:T(8,128)(2,1)S(1)} %bitcast.206, bf16[256,2048]{1,0:T(8,128)(2,1)} %bitcast.18.refs_1_, f32[256,2048]{1,0:T(8,128)S(1)} %copy-done.4, f32[1,2048]{1,0:T(1,128)S(1)} %reshape.401.refs_2_.refs_3_), custom_call_target="tpu_custom_call" | custom-call | tf_op jit(solution)/shard_map/fold_backward/pallas_call | solution.py:521
  448.4 5.7 multiply_reduce_fusion
  454.2 3.1 subtract_convert_fusion.grad_output
  457.3 2.4 collective-permute-done.20
  461.1 2.4 convolution_convert_fusion.6
  467.2 1.7 collective-permute-start.23
  470.7 2.2 copy-done.1
  474.5 21.2 %mixer_backward.1 = (bf16[1024,1536]{1,0:T(8,128)(2,1)S(1)}, f32[64,1024]{1,0:T(8,128)S(1)}) custom-call(s32[1]{0:T(128)} %bitcast.mine, bf16[1024,2048]{1,0:T(8,128)(2,1)S(1)} %copy-done.1, bf16[1024,2048]{1,0:T(8,128)(2,1)S(1)} %copy-done.1, bf16[1024,2048]{1,0:T(8,128)(2,1)S(1)} %copy-done.1, bf16[1024,512]{1,0:T(8,128)(2,1)S(1)} %copy-done.11, ...), custom_call_target="tpu_custom_call" | custom-call | flops 2097152000 | bytes 10485760 | tf_op jit(solution)/shard_map/mixer_backward/pallas_call | solution.py:310
  497.4 11.6 %convolution_convert_fusion = bf16[2048,2048]{1,0:T(8,128)(2,1)} fusion(bf16[1024,2048]{1,0:T(8,128)(2,1)S(1)} %copy-done.19, bf16[1024,512]{1,0:T(8,128)(2,1)S(1)} %copy-done.31, bf16[1024,1536]{1,0:T(8,128)(2,1)S(1)} %get-tuple-element.81), kind=kOutput, calls=%fused_computation.8 | convolution fusion | flops 8602517504 | bytes 16777216 | tf_op jit(solution)/shard_map/dot_general | solution.py:33
  510.1 2.6 pad_maximum_fusion.1
  513.8 12.2 %fusion.46 = f32[1024,2048]{1,0:T(8,128)S(1)} fusion(bf16[1024,2048]{1,0:T(8,128)(2,1)S(1)} %pad_maximum_fusion.1, bf16[2048,2048]{1,0:T(8,128)(2,1)} %all-gather.7.cloned.1.call-done), kind=kOutput, calls=%fused_computation.249 | convolution fusion | flops 8589934592 | bytes 20971520 | tf_op jit(solution)/shard_map/dot_general | solution.py:29
  526.1 2.2 fusion.3
  529.7 12.5 %collective-permute-done.25 = bf16[128,2048]{1,0:T(8,128)(2,1)S(1)} collective-permute-done((bf16[128,2048]{1,0:T(8,128)(2,1)S(1)}, bf16[128,2048]{1,0:T(8,128)(2,1)S(1)}, u32[]{:S(2)}, u32[]{:S(2)}) %collective-permute-start.25) | collective-permute-done | bytes 524320 | tf_op jit(solution)/shard_map/ppermute | solution.py:542
  548.6 2.9 fusion.47
  552.2 15.9 %collective-permute-done.27 = bf16[256,2048]{1,0:T(8,128)(2,1)S(1)} collective-permute-done((bf16[256,2048]{1,0:T(8,128)(2,1)}, bf16[256,2048]{1,0:T(8,128)(2,1)S(1)}, u32[]{:S(2)}, u32[]{:S(2)}) %collective-permute-start.27) | collective-permute-done | bytes 1048608 | tf_op jit(solution)/shard_map/ppermute | solution.py:542
  568.1 2.2 collective-permute-done.28
  572.3 3.8 collective-permute-done.29
  576.9 3.4 convert_add_fusion
  580.3 1.9 copy.70
  582.3 2.2 collective-permute-start.31
  586.1 1.9 collective-permute-done.31
  590.6 3.1 copy.72
  593.7 5.5 fusion.17
  608.2 6.2 collective-permute-done.39
  614.5 7.3 %collective-permute-done.38 = bf16[64,2816]{1,0:T(8,128)(2,1)S(1)} collective-permute-done((bf16[64,2816]{1,0:T(8,128)(2,1)S(1)}, bf16[64,2816]{1,0:T(8,128)(2,1)S(1)}, u32[]{:S(2)}, u32[]{:S(2)}) %collective-permute-start.38) | collective-permute-done | bytes 360480 | tf_op jit(solution)/shard_map/ppermute | solution.py:542
  627.0 1.9 maximum_convert_fusion
  629.7 3.9 collective-permute-done.36
  633.6 4.7 collective-permute-done.35
  (360 shorter events, 103.6 us)
Async XLA Ops:
  7.2 108.7 %all-gather.5.cloned.1.call-start = ((), (), s32[]{:S(2)}) async-start(), calls=%async_computation.4 | async-start | bytes 2359296 | tf_op jit(solution)/shard_map/all_gather | solution.py:734
  7.9 117.9 %all-gather.7.cloned.1.call-start = ((), (), s32[]{:S(2)}) async-start(), calls=%async_computation.5 | async-start | bytes 9437184 | tf_op jit(solution)/shard_map/all_gather | solution.py:738
  15.4 11.1 %collective-permute-start.11 = (bf16[64,2048]{1,0:T(8,128)(2,1)S(1)}, bf16[64,2048]{1,0:T(8,128)(2,1)S(1)}, u32[]{:S(2)}, u32[]{:S(2)}) collective-permute-start(bf16[64,2048]{1,0:T(8,128)(2,1)S(1)} %bitcast.238), channel_id=1, source_target_pairs={{0,24},{8,16},{16,8},{24,0},{1,25},{9,17},{17,9},{25,1},{2,26},{10... | collective-permute-start | bytes 786440 | tf_op jit(solution)/shard_map/ppermute | solution.py:542
  19.5 11.8 %collective-permute-start.10 = (bf16[64,2048]{1,0:T(8,128)(2,1)S(1)}, bf16[64,2048]{1,0:T(8,128)(2,1)S(1)}, u32[]{:S(2)}, u32[]{:S(2)}) collective-permute-start(bf16[64,2048]{1,0:T(8,128)(2,1)S(1)} %bitcast.239), channel_id=1, source_target_pairs={{0,16},{8,24},{16,0},{24,8},{1,17},{9,25},{17,1},{25,9},{2,18},{10... | collective-permute-start | bytes 786440 | tf_op jit(solution)/shard_map/ppermute | solution.py:542
  20.2 11.3 %collective-permute-start.9 = (bf16[64,2048]{1,0:T(8,128)(2,1)S(1)}, bf16[64,2048]{1,0:T(8,128)(2,1)S(1)}, u32[]{:S(2)}, u32[]{:S(2)}) collective-permute-start(bf16[64,2048]{1,0:T(8,128)(2,1)S(1)} %bitcast.240), channel_id=1, source_target_pairs={{0,8},{8,0},{16,24},{24,16},{1,9},{9,1},{17,25},{25,17},{2,10},{10... | collective-permute-start | bytes 786440 | tf_op jit(solution)/shard_map/ppermute | solution.py:542
  33.0 231.6 %all-gather.9.cloned.1.call-start = ((), (), s32[]{:S(2)}) async-start(), calls=%async_computation.6 | async-start | bytes 12976128 | tf_op jit(solution)/shard_map/all_gather | solution.py:740
  37.2 12.3 %collective-permute-start.18 = (bf16[64,2816]{1,0:T(8,128)(2,1)S(1)}, bf16[64,2816]{1,0:T(8,128)(2,1)S(1)}, u32[]{:S(2)}, u32[]{:S(2)}) collective-permute-start(bf16[64,2816]{1,0:T(8,128)(2,1)S(1)} %bitcast.227), channel_id=1, source_target_pairs={{0,24},{8,16},{16,8},{24,0},{1,25},{9,17},{17,9},{25,1},{2,26},{10... | collective-permute-start | bytes 1081352 | tf_op jit(solution)/shard_map/ppermute | solution.py:542
  39.1 17.0 %collective-permute-start.17 = (bf16[64,2816]{1,0:T(8,128)(2,1)S(1)}, bf16[64,2816]{1,0:T(8,128)(2,1)S(1)}, u32[]{:S(2)}, u32[]{:S(2)}) collective-permute-start(bf16[64,2816]{1,0:T(8,128)(2,1)S(1)} %bitcast.228), channel_id=1, source_target_pairs={{0,16},{8,24},{16,0},{24,8},{1,17},{9,25},{17,1},{25,9},{2,18},{10... | collective-permute-start | bytes 1081352 | tf_op jit(solution)/shard_map/ppermute | solution.py:542
  40.4 16.0 %collective-permute-start.16 = (bf16[64,2816]{1,0:T(8,128)(2,1)S(1)}, bf16[64,2816]{1,0:T(8,128)(2,1)S(1)}, u32[]{:S(2)}, u32[]{:S(2)}) collective-permute-start(bf16[64,2816]{1,0:T(8,128)(2,1)S(1)} %bitcast.229), channel_id=1, source_target_pairs={{0,8},{8,0},{16,24},{24,16},{1,9},{9,1},{17,25},{25,17},{2,10},{10... | collective-permute-start | bytes 1081352 | tf_op jit(solution)/shard_map/ppermute | solution.py:542
  56.8 16.0 %copy-start.2 = (bf16[1,256,2048]{2,1,0:T(8,128)(2,1)S(1)}, bf16[1,256,2048]{2,1,0:T(8,128)(2,1)}, u32[]{:S(2)}) copy-start(bf16[1,256,2048]{2,1,0:T(8,128)(2,1)} %param.17) | copy-start | bytes 3145732
  58.1 239.0 %all-gather.11.cloned.1.call-start = ((), (), s32[]{:S(2)}) async-start(), calls=%async_computation.7 | async-start | bytes 6488064 | tf_op jit(solution)/shard_map/all_gather | solution.py:741
  58.9 1.2 collective-permute-start.4
  60.1 3.8 collective-permute-start.5
  64.0 7.1 %collective-permute-start.6 = (bf16[4,1608]{1,0:T(4,128)(2,1)S(1)}, bf16[4,1608]{1,0:T(4,128)(2,1)S(1)}, u32[]{:S(2)}, u32[]{:S(2)}) collective-permute-start(bf16[4,1608]{1,0:T(4,128)(2,1)S(1)} %pad_maximum_fusion.27), channel_id=1, source_target_pairs={{0,4},{1,5},{2,6},{3,7},{4,0},{5,1},{6,2},{7,3},{8,12},{9,13},{10,... | collective-permute-start | bytes 38600 | tf_op jit(solution)/shard_map/ppermute | solution.py:580
  71.2 6.8 %collective-permute-start.7 = (bf16[8,1608]{1,0:T(8,128)(2,1)S(1)}, bf16[8,1608]{1,0:T(8,128)(2,1)S(1)}, u32[]{:S(2)}, u32[]{:S(2)}) collective-permute-start(bf16[8,1608]{1,0:T(8,128)(2,1)S(1)} %pad_maximum_fusion.26), channel_id=1, source_target_pairs={{0,8},{8,0},{16,24},{24,16},{1,9},{9,1},{17,25},{25,17},{2,10},{10... | collective-permute-start | bytes 77192 | tf_op jit(solution)/shard_map/ppermute | solution.py:580
  75.9 28.9 %collective-permute-start = (bf16[256,2048]{1,0:T(8,128)(2,1)S(1)}, bf16[256,2048]{1,0:T(8,128)(2,1)}, u32[]{:S(2)}, u32[]{:S(2)}) collective-permute-start(bf16[256,2048]{1,0:T(8,128)(2,1)S(1)} %copy.61), channel_id=1, source_target_pairs={{0,8},{8,0},{16,24},{24,16},{1,9},{9,1},{17,25},{25,17},{2,10},{10... | collective-permute-start | bytes 3145736 | tf_op jit(solution)/shard_map/ppermute | solution.py:542
  76.5 23.7 %collective-permute-start.1 = (bf16[256,2048]{1,0:T(8,128)(2,1)S(1)}, bf16[256,2048]{1,0:T(8,128)(2,1)}, u32[]{:S(2)}, u32[]{:S(2)}) collective-permute-start(bf16[256,2048]{1,0:T(8,128)(2,1)S(1)} %copy.61), channel_id=1, source_target_pairs={{0,16},{8,24},{16,0},{24,8},{1,17},{9,25},{17,1},{25,9},{2,18},{10... | collective-permute-start | bytes 3145736 | tf_op jit(solution)/shard_map/ppermute | solution.py:542
  78.0 20.7 %collective-permute-start.8 = (bf16[16,1608]{1,0:T(8,128)(2,1)S(1)}, bf16[16,1608]{1,0:T(8,128)(2,1)S(1)}, u32[]{:S(2)}, u32[]{:S(2)}) collective-permute-start(bf16[16,1608]{1,0:T(8,128)(2,1)S(1)} %pad_maximum_fusion.25), channel_id=1, source_target_pairs={{0,16},{8,24},{16,0},{24,8},{1,17},{9,25},{17,1},{25,9},{2,18},{10... | collective-permute-start | bytes 154376 | tf_op jit(solution)/shard_map/ppermute | solution.py:580
  102.1 9.5 %collective-permute-start.2 = (bf16[128,2048]{1,0:T(8,128)(2,1)}, bf16[128,2048]{1,0:T(8,128)(2,1)}, u32[]{:S(2)}, u32[]{:S(2)}) collective-permute-start(bf16[128,2048]{1,0:T(8,128)(2,1)} %slice.292), channel_id=1, source_target_pairs={{0,8},{8,0},{16,24},{24,16},{1,9},{9,1},{17,25},{25,17},{2,10},{10... | collective-permute-start | bytes 1572872 | tf_op jit(solution)/shard_map/ppermute | solution.py:542
  104.4 16.0 %copy-start.36 = (bf16[16,2048]{1,0:T(8,128)(2,1)}, bf16[16,2048]{1,0:T(8,128)(2,1)S(1)}, u32[]{:S(2)}) copy-start(bf16[16,2048]{1,0:T(8,128)(2,1)S(1)} %reshape.368) | copy-start | bytes 196612
  104.5 17.1 %copy-start.46 = (bf16[256,16]{1,0:T(8,128)(2,1)}, bf16[256,16]{1,0:T(8,128)(2,1)S(1)}, u32[]{:S(2)}) copy-start(bf16[256,16]{1,0:T(8,128)(2,1)S(1)} %reshape.365) | copy-start | bytes 24580
  104.7 260.6 %reduce-scatter.5.cloned.1.call-start = ((), (), s32[]{:S(2)}) async-start(), calls=%async_computation.8 | async-start | bytes 6488064 | tf_op jit(solution)/shard_map/reduce_scatter | solution.py:833
  105.8 9.2 %collective-permute-start.3 = (bf16[128,2048]{1,0:T(8,128)(2,1)S(1)}, bf16[128,2048]{1,0:T(8,128)(2,1)S(1)}, u32[]{:S(2)}, u32[]{:S(2)}) collective-permute-start(bf16[128,2048]{1,0:T(8,128)(2,1)S(1)} %slice.293), channel_id=1, source_target_pairs={{0,16},{8,24},{16,0},{24,8},{1,17},{9,25},{17,1},{25,9},{2,18},{10... | collective-permute-start | bytes 1572872 | tf_op jit(solution)/shard_map/ppermute | solution.py:542
  125.8 15.4 %copy-start.6 = (f32[128,1024]{1,0:T(8,128)S(1)}, f32[128,1024]{1,0:T(8,128)}, u32[]{:S(2)}) copy-start(f32[128,1024]{1,0:T(8,128)} %pad_maximum_fusion.21.rate) | copy-start | bytes 1572868
  125.8 34.4 %collective-permute-start.12 = (bf16[256,2048]{1,0:T(8,128)(2,1)}, bf16[256,2048]{1,0:T(8,128)(2,1)S(1)}, u32[]{:S(2)}, u32[]{:S(2)}) collective-permute-start(bf16[256,2048]{1,0:T(8,128)(2,1)} %bitcast.18.refs_1_), channel_id=1, source_target_pairs={{0,8},{8,0},{16,24},{24,16},{1,9},{9,1},{17,25},{25,17},{2,10},{10... | collective-permute-start | bytes 3145736 | tf_op jit(solution)/shard_map/ppermute | solution.py:542
  127.3 30.8 %collective-permute-start.13 = (bf16[256,2048]{1,0:T(8,128)(2,1)}, bf16[256,2048]{1,0:T(8,128)(2,1)S(1)}, u32[]{:S(2)}, u32[]{:S(2)}) collective-permute-start(bf16[256,2048]{1,0:T(8,128)(2,1)} %bitcast.18.refs_1_), channel_id=1, source_target_pairs={{0,16},{8,24},{16,0},{24,8},{1,17},{9,25},{17,1},{25,9},{2,18},{10... | collective-permute-start | bytes 3145736 | tf_op jit(solution)/shard_map/ppermute | solution.py:542
  141.2 12.0 %copy-start = (bf16[1024,2048]{1,0:T(8,128)(2,1)}, bf16[1024,2048]{1,0:T(8,128)(2,1)S(1)}, u32[]{:S(2)}) copy-start(bf16[1024,2048]{1,0:T(8,128)(2,1)S(1)} %get-tuple-element.241.query.key.value) | copy-start | bytes 12582916
  141.2 12.2 %copy-start.28 = (f32[1024,2048]{1,0:T(8,128)}, f32[1024,2048]{1,0:T(8,128)S(1)}, u32[]{:S(2)}) copy-start(f32[1024,2048]{1,0:T(8,128)S(1)} %get-tuple-element.242) | copy-start | bytes 25165828
  158.1 13.6 %collective-permute-start.14 = (bf16[128,2048]{1,0:T(8,128)(2,1)S(1)}, bf16[128,2048]{1,0:T(8,128)(2,1)S(1)}, u32[]{:S(2)}, u32[]{:S(2)}) collective-permute-start(bf16[128,2048]{1,0:T(8,128)(2,1)S(1)} %slice.296), channel_id=1, source_target_pairs={{0,8},{8,0},{16,24},{24,16},{1,9},{9,1},{17,25},{25,17},{2,10},{10... | collective-permute-start | bytes 1572872 | tf_op jit(solution)/shard_map/ppermute | solution.py:542
  160.2 13.3 %collective-permute-start.15 = (bf16[128,2048]{1,0:T(8,128)(2,1)S(1)}, bf16[128,2048]{1,0:T(8,128)(2,1)S(1)}, u32[]{:S(2)}, u32[]{:S(2)}) collective-permute-start(bf16[128,2048]{1,0:T(8,128)(2,1)S(1)} %slice.297), channel_id=1, source_target_pairs={{0,16},{8,24},{16,0},{24,8},{1,17},{9,25},{17,1},{25,9},{2,18},{10... | collective-permute-start | bytes 1572872 | tf_op jit(solution)/shard_map/ppermute | solution.py:542
  297.1 173.3 %reduce-scatter.7.cloned.1.call-start = ((), (), s32[]{:S(2)}) async-start(), calls=%async_computation.9 | async-start | bytes 7208960 | tf_op jit(solution)/shard_map/reduce_scatter | solution.py:633
  314.1 17.8 %copy-start.10 = (bf16[4,256,2048]{2,1,0:T(8,128)(2,1)S(1)}, bf16[4,256,2048]{2,1,0:T(8,128)(2,1)}, u32[]{:S(2)}) copy-start(bf16[4,256,2048]{2,1,0:T(8,128)(2,1)} %copy-done.9) | copy-start | bytes 12582916
  343.7 12.9 %collective-permute-start.19 = (bf16[1024,2816]{1,0:T(8,128)(2,1)}, bf16[1024,2816]{1,0:T(8,128)(2,1)S(1)}, u32[]{:S(2)}, u32[]{:S(2)}) collective-permute-start(bf16[1024,2816]{1,0:T(8,128)(2,1)} %convolution_convert_fusion.2), channel_id=1, source_target_pairs={{0,1},{1,0},{2,3},{3,2},{4,5},{5,4},{6,7},{7,6},{8,9},{9,8},{10,11... | collective-permute-start | bytes 17301512 | tf_op jit(solution)/shard_map/ppermute | solution.py:580
  345.6 11.1 %copy-start.60 = (bf16[1024,1408]{1,0:T(8,128)(2,1)S(1)}, bf16[1024,1408]{1,0:T(8,128)(2,1)}, u32[]{:S(2)}) copy-start(bf16[1024,1408]{1,0:T(8,128)(2,1)} %get-tuple-element.133) | copy-start | bytes 8650756
  365.3 143.6 %reduce-scatter.9.cloned.1.call-start = ((), (), s32[]{:S(2)}) async-start(), calls=%async_computation.10 | async-start | bytes 1310720 | tf_op jit(solution)/shard_map/reduce_scatter | solution.py:633
  369.3 76.7 %copy-start.25 = (bf16[1024,2048]{1,0:T(8,128)(2,1)S(1)}, bf16[1024,2048]{1,0:T(8,128)(2,1)}, u32[]{:S(2)}) copy-start(bf16[1024,2048]{1,0:T(8,128)(2,1)} %convolution_convert_fusion.4) | copy-start | bytes 12582916
  446.3 13.4 %collective-permute-start.20 = (bf16[128,2048]{1,0:T(8,128)(2,1)S(1)}, bf16[128,2048]{1,0:T(8,128)(2,1)S(1)}, u32[]{:S(2)}, u32[]{:S(2)}) collective-permute-start(bf16[128,2048]{1,0:T(8,128)(2,1)S(1)} %get-tuple-element.147), channel_id=1, source_target_pairs={{0,8},{8,0},{16,24},{24,16},{1,9},{9,1},{17,25},{25,17},{2,10},{10... | collective-permute-start | bytes 1572872 | tf_op jit(solution)/shard_map/ppermute | solution.py:542
  447.8 13.3 %collective-permute-start.21 = (bf16[128,2048]{1,0:T(8,128)(2,1)S(1)}, bf16[128,2048]{1,0:T(8,128)(2,1)S(1)}, u32[]{:S(2)}, u32[]{:S(2)}) collective-permute-start(bf16[128,2048]{1,0:T(8,128)(2,1)S(1)} %get-tuple-element.146), channel_id=1, source_target_pairs={{0,16},{8,24},{16,0},{24,8},{1,17},{9,25},{17,1},{25,9},{2,18},{10... | collective-permute-start | bytes 1572872 | tf_op jit(solution)/shard_map/ppermute | solution.py:542
  464.1 4.7 collective-permute-start.24
  465.7 30.0 %collective-permute-start.22 = (bf16[256,2048]{1,0:T(8,128)(2,1)}, bf16[256,2048]{1,0:T(8,128)(2,1)}, u32[]{:S(2)}, u32[]{:S(2)}) collective-permute-start(bf16[256,2048]{1,0:T(8,128)(2,1)} %pad_maximum_fusion.14), channel_id=1, source_target_pairs={{0,8},{8,0},{16,24},{24,16},{1,9},{9,1},{17,25},{25,17},{2,10},{10... | collective-permute-start | bytes 3145736 | tf_op jit(solution)/shard_map/ppermute | solution.py:542
  467.2 28.6 %collective-permute-start.23 = (bf16[256,2048]{1,0:T(8,128)(2,1)}, bf16[256,2048]{1,0:T(8,128)(2,1)}, u32[]{:S(2)}, u32[]{:S(2)}) collective-permute-start(bf16[256,2048]{1,0:T(8,128)(2,1)} %pad_maximum_fusion.15), channel_id=1, source_target_pairs={{0,16},{8,24},{16,0},{24,8},{1,17},{9,25},{17,1},{25,9},{2,18},{10... | collective-permute-start | bytes 3145736 | tf_op jit(solution)/shard_map/ppermute | solution.py:542
  470.4 151.7 %reduce-scatter.11.cloned.1.call-start = ((), (), s32[]{:S(2)}) async-start(), calls=%async_computation.11 | async-start | bytes 9437184 | tf_op jit(solution)/shard_map/reduce_scatter | solution.py:889
  474.5 22.9 %copy-start.19 = (bf16[1024,2048]{1,0:T(8,128)(2,1)S(1)}, bf16[1024,2048]{1,0:T(8,128)(2,1)}, u32[]{:S(2)}) copy-start(bf16[1024,2048]{1,0:T(8,128)(2,1)} %copy-done.18) | copy-start | bytes 12582916
  474.5 22.9 %copy-start.31 = (bf16[1024,512]{1,0:T(8,128)(2,1)S(1)}, bf16[1024,512]{1,0:T(8,128)(2,1)}, u32[]{:S(2)}) copy-start(bf16[1024,512]{1,0:T(8,128)(2,1)} %get-tuple-element.134) | copy-start | bytes 3145732
  513.8 12.2 %copy-start.21 = (bf16[1024,2048]{1,0:T(8,128)(2,1)S(1)}, bf16[1024,2048]{1,0:T(8,128)(2,1)}, u32[]{:S(2)}) copy-start(bf16[1024,2048]{1,0:T(8,128)(2,1)} %constant_dynamic-update-slice_fusion) | copy-start | bytes 12582916
  513.8 12.2 %copy-start.37 = (bf16[16,2048]{1,0:T(8,128)(2,1)S(1)}, bf16[16,2048]{1,0:T(8,128)(2,1)}, u32[]{:S(2)}) copy-start(bf16[16,2048]{1,0:T(8,128)(2,1)} %copy-done.36) | copy-start | bytes 196612
  513.8 12.2 %copy-start.48 = (f32[1024]{0:T(1024)S(1)}, f32[1024]{0:T(1024)}, u32[]{:S(2)}) copy-start(f32[1024]{0:T(1024)} %copy-done.47) | copy-start | bytes 12292
  528.2 14.4 %copy-start.22 = (bf16[1024,2048]{1,0:T(8,128)(2,1)}, bf16[1024,2048]{1,0:T(8,128)(2,1)S(1)}, u32[]{:S(2)}) copy-start(bf16[1024,2048]{1,0:T(8,128)(2,1)S(1)} %get-tuple-element.136) | copy-start | bytes 12582916
  528.4 13.8 %collective-permute-start.25 = (bf16[128,2048]{1,0:T(8,128)(2,1)S(1)}, bf16[128,2048]{1,0:T(8,128)(2,1)S(1)}, u32[]{:S(2)}, u32[]{:S(2)}) collective-permute-start(bf16[128,2048]{1,0:T(8,128)(2,1)S(1)} %get-tuple-element.141), channel_id=1, source_target_pairs={{0,8},{8,0},{16,24},{24,16},{1,9},{9,1},{17,25},{25,17},{2,10},{10... | collective-permute-start | bytes 1572872 | tf_op jit(solution)/shard_map/ppermute | solution.py:542
  528.5 13.8 %collective-permute-start.26 = (bf16[128,2048]{1,0:T(8,128)(2,1)S(1)}, bf16[128,2048]{1,0:T(8,128)(2,1)S(1)}, u32[]{:S(2)}, u32[]{:S(2)}) collective-permute-start(bf16[128,2048]{1,0:T(8,128)(2,1)S(1)} %get-tuple-element.140), channel_id=1, source_target_pairs={{0,16},{8,24},{16,0},{24,8},{1,17},{9,25},{17,1},{25,9},{2,18},{10... | collective-permute-start | bytes 1572872 | tf_op jit(solution)/shard_map/ppermute | solution.py:542
  543.7 24.4 %collective-permute-start.27 = (bf16[256,2048]{1,0:T(8,128)(2,1)}, bf16[256,2048]{1,0:T(8,128)(2,1)S(1)}, u32[]{:S(2)}, u32[]{:S(2)}) collective-permute-start(bf16[256,2048]{1,0:T(8,128)(2,1)} %pad_maximum_fusion.18), channel_id=1, source_target_pairs={{0,8},{8,0},{16,24},{24,16},{1,9},{9,1},{17,25},{25,17},{2,10},{10... | collective-permute-start | bytes 3145736 | tf_op jit(solution)/shard_map/ppermute | solution.py:542
  546.5 23.9 %collective-permute-start.28 = (bf16[256,2048]{1,0:T(8,128)(2,1)}, bf16[256,2048]{1,0:T(8,128)(2,1)}, u32[]{:S(2)}, u32[]{:S(2)}) collective-permute-start(bf16[256,2048]{1,0:T(8,128)(2,1)} %pad_maximum_fusion.19), channel_id=1, source_target_pairs={{0,16},{8,24},{16,0},{24,8},{1,17},{9,25},{17,1},{25,9},{2,18},{10... | collective-permute-start | bytes 3145736 | tf_op jit(solution)/shard_map/ppermute | solution.py:542
  551.4 20.8 %copy-start.39 = (f32[32,64]{1,0:T(8,128)S(1)}, f32[32,64]{1,0:T(8,128)}, u32[]{:S(2)}) copy-start(f32[32,64]{1,0:T(8,128)} %copy-done.38) | copy-start | bytes 24580
  571.6 4.6 collective-permute-start.29
  576.2 6.1 collective-permute-start.30
  582.3 5.8 collective-permute-start.31
  588.1 5.5 collective-permute-start.32
  593.7 5.6 collective-permute-start.33
  602.2 12.2 %collective-permute-start.39 = (bf16[64,2816]{1,0:T(8,128)(2,1)S(1)}, bf16[64,2816]{1,0:T(8,128)(2,1)S(1)}, u32[]{:S(2)}, u32[]{:S(2)}) collective-permute-start(bf16[64,2816]{1,0:T(8,128)(2,1)S(1)} %get-tuple-element.174), channel_id=1, source_target_pairs={{0,24},{8,16},{16,8},{24,0},{1,25},{9,17},{17,9},{25,1},{2,26},{10... | collective-permute-start | bytes 1081352 | tf_op jit(solution)/shard_map/ppermute | solution.py:542
  603.8 17.9 %collective-permute-start.38 = (bf16[64,2816]{1,0:T(8,128)(2,1)S(1)}, bf16[64,2816]{1,0:T(8,128)(2,1)S(1)}, u32[]{:S(2)}, u32[]{:S(2)}) collective-permute-start(bf16[64,2816]{1,0:T(8,128)(2,1)S(1)} %get-tuple-element.175), channel_id=1, source_target_pairs={{0,16},{8,24},{16,0},{24,8},{1,17},{9,25},{17,1},{25,9},{2,18},{10... | collective-permute-start | bytes 1081352 | tf_op jit(solution)/shard_map/ppermute | solution.py:542
  605.1 16.6 %collective-permute-start.37 = (bf16[64,2816]{1,0:T(8,128)(2,1)S(1)}, bf16[64,2816]{1,0:T(8,128)(2,1)S(1)}, u32[]{:S(2)}, u32[]{:S(2)}) collective-permute-start(bf16[64,2816]{1,0:T(8,128)(2,1)S(1)} %get-tuple-element.176), channel_id=1, source_target_pairs={{0,8},{8,0},{16,24},{24,16},{1,9},{9,1},{17,25},{25,17},{2,10},{10... | collective-permute-start | bytes 1081352 | tf_op jit(solution)/shard_map/ppermute | solution.py:542
  623.4 10.2 %collective-permute-start.36 = (bf16[64,2048]{1,0:T(8,128)(2,1)S(1)}, bf16[64,2048]{1,0:T(8,128)(2,1)S(1)}, u32[]{:S(2)}, u32[]{:S(2)}) collective-permute-start(bf16[64,2048]{1,0:T(8,128)(2,1)S(1)} %get-tuple-element.202), channel_id=1, source_target_pairs={{0,24},{8,16},{16,8},{24,0},{1,25},{9,17},{17,9},{25,1},{2,26},{10... | collective-permute-start | bytes 786440 | tf_op jit(solution)/shard_map/ppermute | solution.py:542
  625.0 13.3 %collective-permute-start.35 = (bf16[64,2048]{1,0:T(8,128)(2,1)S(1)}, bf16[64,2048]{1,0:T(8,128)(2,1)S(1)}, u32[]{:S(2)}, u32[]{:S(2)}) collective-permute-start(bf16[64,2048]{1,0:T(8,128)(2,1)S(1)} %get-tuple-element.203), channel_id=1, source_target_pairs={{0,16},{8,24},{16,0},{24,8},{1,17},{9,25},{17,1},{25,9},{2,18},{10... | collective-permute-start | bytes 786440 | tf_op jit(solution)/shard_map/ppermute | solution.py:542
  626.3 11.9 %collective-permute-start.34 = (bf16[64,2048]{1,0:T(8,128)(2,1)S(1)}, bf16[64,2048]{1,0:T(8,128)(2,1)S(1)}, u32[]{:S(2)}, u32[]{:S(2)}) collective-permute-start(bf16[64,2048]{1,0:T(8,128)(2,1)S(1)} %get-tuple-element.204), channel_id=1, source_target_pairs={{0,8},{8,0},{16,24},{24,16},{1,9},{9,1},{17,25},{25,17},{2,10},{10... | collective-permute-start | bytes 786440 | tf_op jit(solution)/shard_map/ppermute | solution.py:542
  (45 other events, 138.6 us)
Sparse Core Ops, SparseCore 0:
  9.6 31.7 all-gather.4
  43.6 82.1 all-gather.6
  128.0 106.4 all-gather.8
  236.0 58.7 all-gather.10
  297.2 64.8 reduce-scatter.4
  365.4 102.2 reduce-scatter.6
  470.5 27.1 reduce-scatter.8
  509.1 90.3 reduce-scatter.10

commit v13 on v12

--- a/solution.py
+++ b/solution.py
@@ -893,8 +893,9 @@
     grad_normed = dot_nt(after(grad_pre, term_pre), w_mixer) + dot_nn(grad_reduced, w_squeeze)
     term_mixer = restored(jnp.sum(grad_normed * plain_one, axis=0))
     term_squeeze = restored(dot_tn(grad_reduced, normed))
-    grad_normed, _, (term_mixer, term_squeeze) = scattered(
-        grad_normed.astype(BF16), ring, term_bias, (term_mixer, term_squeeze)
+    feed_share = exchanged(after(feed_sum, term_pre).reshape(ring, own, 2 * hidden_part), mine, ring)
+    grad_normed, feed_share, (term_mixer, term_squeeze) = scattered(
+        grad_normed.astype(BF16), ring, feed_share, (term_mixer, term_squeeze)
     )
     grad_normed = restored(grad_normed)
     inputs_own = input_own.astype(F32)
@@ -915,7 +916,6 @@
     query_share, key_share, value_share, swish_share = (
         joined_columns(pre_share, at * part, part) for at in range(4)
     )
-    feed_share = exchanged(after(feed_sum, term_pre).reshape(ring, own, 2 * hidden_part), mine, ring)
     gate_share = joined_columns(feed_share, 0, hidden_part)
     up_share = joined_columns(feed_share, hidden_part, hidden_part)
 

time: 656 us -> 660 us (level)
  waiting for transfers between devices: 133 us -> 118 us
  local copies, waits for them, and re-layouts: 72.4 us -> 83.6 us
    ppermute x28, waiting for transfers between devices: 97.5 us -> 89.7 us  [swapped(): return lax.ppermute(block, 'seq', [(i, i ^ by) for i in range(ring)])]
    unnamed x148 -> x162, local copies, waits for them, and re-layouts: 37.9 us -> 40.4 us
  transfers between devices with their start and end apart: 48 -> 48, of which waited for: 27 -> 25; matrix products, arithmetic and copies ran while one was open for 36% -> 37% of each run, Pallas kernels for 30% -> 30%
where the time goes in v13:
time: 660 us; the launch traced here: 651 us
  Pallas kernels  198 us (30%)
  matrix products  142 us (22%)
  waiting for transfers between devices  118 us (18%)
  local copies, waits for them, and re-layouts  83.6 us (13%)
  other arithmetic  47.4 us (7%)
  starting transfers between devices  46.4 us (7%)
  between operations  16.1 us (2%)
    pallas_call x2, Pallas kernels, fold(): pl.pallas_call(functools.partial(fold_kernel, finish, len(given)), out_sh...  165 us
    ppermute x28, waiting for transfers between devices, swapped(): return lax.ppermute(block, 'seq', [(i, i ^ by) for i in range(ring)])  89.7 us
    dot_general x6, matrix products, dot_nt(): lax.dot_general(left, right, (((1,), (1,)), ((), ())), preferred_element_...  52.6 us
    dot_general x6, matrix products, dot_nn(): lax.dot_general(left, right, (((1,), (0,)), ((), ())), preferred_element_...  45.3 us
    dot_general x7, matrix products, dot_tn(): lax.dot_general(left, right, (((0,), (0,)), ((), ())), preferred_element_...  43.8 us
    unnamed x162, local copies, waits for them, and re-layouts  40.4 us
    ppermute x28, starting transfers between devices, swapped(): return lax.ppermute(block, 'seq', [(i, i ^ by) for i in range(ring)])  32 us
    ppermute x12, waiting for transfers between devices, flipped(): lax.ppermute(block, axis, [(i, i ^ by) for i in range(lax.axis_size(axis))])  27.8 us
  transfers between devices with their start and end apart: 48, of which 25 were waited for; matrix products, arithmetic and copies ran while one was open for 37% of the time, Pallas kernels for 30%

profile of v13, /device:TPU:0, one launch (start us, length us, event | category | flops | bytes accessed | tf_op | source)
XLA Modules:
  0.0 651.5 jit_solution(15250382606296070393)
XLA Ops:
  13.1 2.2 constant_dynamic-slice_fusion.22
  15.4 4.0 collective-permute-start.11
  20.5 6.0 collective-permute-done.11
  26.5 4.7 collective-permute-done.10
  34.2 3.0 constant_dynamic-slice_fusion.13
  37.2 1.8 collective-permute-start.18
  41.0 8.5 %collective-permute-done.18 = bf16[64,2816]{1,0:T(8,128)(2,1)S(1)} collective-permute-done((bf16[64,2816]{1,0:T(8,128)(2,1)S(1)}, bf16[64,2816]{1,0:T(8,128)(2,1)S(1)}, u32[]{:S(2)}, u32[]{:S(2)}) %collective-permute-start.18) | collective-permute-done | bytes 360480 | tf_op jit(solution)/shard_map/ppermute | solution.py:542
  49.5 6.5 %collective-permute-done.17 = bf16[64,2816]{1,0:T(8,128)(2,1)S(1)} collective-permute-done((bf16[64,2816]{1,0:T(8,128)(2,1)S(1)}, bf16[64,2816]{1,0:T(8,128)(2,1)S(1)}, u32[]{:S(2)}, u32[]{:S(2)}) %collective-permute-start.17) | collective-permute-done | bytes 360480 | tf_op jit(solution)/shard_map/ppermute | solution.py:542
  61.8 2.2 collective-permute-done.5
  64.0 2.5 collective-permute-start.6
  66.6 4.6 collective-permute-done.6
  79.7 19.1 %collective-permute-done.8 = bf16[16,1608]{1,0:T(8,128)(2,1)S(1)} collective-permute-done((bf16[16,1608]{1,0:T(8,128)(2,1)S(1)}, bf16[16,1608]{1,0:T(8,128)(2,1)S(1)}, u32[]{:S(2)}, u32[]{:S(2)}) %collective-permute-start.8) | collective-permute-done | bytes 51488 | tf_op jit(solution)/shard_map/ppermute | solution.py:580
  100.2 1.9 slice.292
  106.5 2.3 constant_dynamic-update-slice_fusion.3
  108.8 2.4 constant_dynamic-update-slice_fusion.2
  111.6 1.9 constant_dynamic-update-slice_fusion.1
  115.9 3.2 fusion.4
  120.8 2.0 copy-done.19
  128.7 12.5 %fusion.44 = (bf16[1024,2048]{1,0:T(8,128)(2,1)S(1)}, f32[1024,2048]{1,0:T(8,128)S(1)}) fusion(bf16[1024,2048]{1,0:T(8,128)(2,1)} %copy-done.19, bf16[2048,2048]{1,0:T(8,128)(2,1)} %all-gather.7.cloned.1.call-done), kind=kOutput, calls=%fused_computation.252 | convolution fusion | flops 8592031744 | bytes 25165824 | tf_op jit(solution)/shard_map/dot_general | solution.py:25
  141.3 11.9 %mixer_forward.1 = (f32[1024,512]{1,0:T(8,128)S(1)}, f32[128,1024]{1,0:T(8,128)S(1)}, f32[8,128,512]{2,1,0:T(8,128)S(1)}) custom-call(s32[1]{0:T(128)} %bitcast.mine, bf16[1024,2048]{1,0:T(8,128)(2,1)S(1)} %get-tuple-element.247.query.key.value, bf16[1024,2048]{1,0:T(8,128)(2,1)S(1)} %get-tuple-element.247.query.key.value, ...), custom_call_target="tpu_custom_call" | custom-call | flops 1048576000 | bytes 6291456 | tf_op jit(solution)/shard_map/mixer_forward/pallas_call | solution.py:285
  155.7 2.3 convolution_convert_fusion.5
  161.2 10.5 %collective-permute-done.14 = bf16[128,2048]{1,0:T(8,128)(2,1)S(1)} collective-permute-done((bf16[128,2048]{1,0:T(8,128)(2,1)S(1)}, bf16[128,2048]{1,0:T(8,128)(2,1)S(1)}, u32[]{:S(2)}, u32[]{:S(2)}) %collective-permute-start.14) | collective-permute-done | bytes 524320 | tf_op jit(solution)/shard_map/ppermute | solution.py:542
  171.8 1.7 collective-permute-done.15
  173.6 2.0 copy-done.44
  175.5 87.9 %fold_forward.1 = (bf16[4,256,2048]{2,1,0:T(8,128)(2,1)S(1)}, f32[256,2048]{1,0:T(8,128)S(1)}) custom-call(bf16[4,256,2048]{2,1,0:T(8,128)(2,1)S(1)} %bitcast.205, bf16[256,2048]{1,0:T(8,128)(2,1)S(1)} %bitcast.204, f32[1,2048]{1,0:T(1,128)S(1)} %reshape.401.refs_2_.refs_3_), custom_call_target="tpu_custom_call" | custom-call | tf_op jit(solution)/shard_map/fold_forward/pallas_call | solution.py:521
  264.9 2.1 copy-done.9
  267.0 17.3 %fusion.45 = f32[1024,2816]{1,0:T(8,128)S(1)} fusion(bf16[1024,2048]{1,0:T(8,128)(2,1)} %bitcast.207, bf16[2048,2816]{1,0:T(8,128)(2,1)} %all-gather.9.cloned.1.call-done), kind=kOutput, calls=%fused_computation.253 | convolution fusion | flops 11811160064 | bytes 27262976 | tf_op jit(solution)/shard_map/dot_general | solution.py:25
  284.3 1.8 multiply_convert_fusion.2
  286.2 3.5 copy-done.25
  291.2 8.1 %convolution_convert_fusion.1 = bf16[1408,2048]{1,0:T(8,128)(2,1)} fusion(bf16[1024,1408]{1,0:T(8,128)(2,1)S(1)} %multiply_convert_fusion.2, bf16[1024,2048]{1,0:T(8,128)(2,1)S(1)} %copy-done.45), kind=kOutput, calls=%fused_computation.9 | convolution fusion | flops 5908463616 | bytes 12845056 | tf_op jit(solution)/shard_map/dot_general | solution.py:33
  299.4 15.4 %multiply_convert_fusion.1 = (bf16[1024,1408]{1,0:T(8,128)(2,1)S(1)}, bf16[1024,1408]{1,0:T(8,128)(2,1)}) fusion(f32[1024,2816]{1,0:T(8,128)} %copy-done.25, bf16[1024,2048]{1,0:T(8,128)(2,1)} %copy-done.44, bf16[1408,2048]{1,0:T(8,128)(2,1)} %all-gather.11.cloned.1.call-done), kind=kOutput, calls=%fused_computation.12 | convolution fusion | flops 5924323328 | bytes 27262976 | tf_op jit(solution)/shard_map/dot_general | solution.py:29
  316.4 17.8 %convolution_convert_fusion.3 = bf16[1024,2048]{1,0:T(8,128)(2,1)} fusion(bf16[2048,2816]{1,0:T(8,128)(2,1)} %all-gather.9.cloned.1.call-done, bf16[1024,1408]{1,0:T(8,128)(2,1)} %get-tuple-element.135, bf16[1024,1408]{1,0:T(8,128)(2,1)S(1)} %get-tuple-element.134), kind=kOutput, calls=%fused_computation.19 | convolution fusion | flops 11824791552 | bytes 21495808 | tf_op jit(solution)/shard_map/dot_general | solution.py:29
  334.5 11.5 %convolution_convert_fusion.2 = bf16[1024,2816]{1,0:T(8,128)(2,1)} fusion(pred[]{:T(512)S(6)} %eq.86, bf16[1024,1408]{1,0:T(8,128)(2,1)} %get-tuple-element.135, bf16[1024,1408]{1,0:T(8,128)(2,1)} %copy-done.65, bf16[1024,256]{1,0:T(8,128)(2,1)S(1)} %get-tuple-element.152, bf16[1024,256]{1,0:T(8,128)(2,1)S(1)} %get-tuple-element.153, ...), kind=kOutput, calls=%fused_computation.16 | convolution fusion | flops 5937823744 | bytes 15728641 | tf_op jit(solution)/shard_map/dot_general | solution.py:33
  348.0 11.1 %convolution_convert_fusion.4 = bf16[1024,2048]{1,0:T(8,128)(2,1)} fusion(bf16[1024,1408]{1,0:T(8,128)(2,1)S(1)} %copy-done.29, bf16[1408,2048]{1,0:T(8,128)(2,1)} %all-gather.11.cloned.1.call-done), kind=kOutput, calls=%fused_computation.20 | convolution fusion | flops 5907677184 | bytes 12845056 | tf_op jit(solution)/shard_map/dot_general | solution.py:25
  359.0 8.6 %add_convert_fusion = bf16[1024,2816]{1,0:T(8,128)(2,1)} fusion(bf16[1024,2816]{1,0:T(8,128)(2,1)S(1)} %collective-permute-done.19, bf16[1024,1024]{1,0:T(8,128)(2,1)S(1)} %broadcast_select_fusion, bf16[1024,1408]{1,0:T(8,128)(2,1)S(1)} %copy-done.67, bf16[1024,1408]{1,0:T(8,128)(2,1)S(1)} %copy-done.66), kind=kOutput, calls=%fused_computation | convolution fusion | flops 5925765120 | bytes 19398656 | tf_op jit(solution)/shard_map/dot_general | solution.py:33
  369.5 2.2 copy-done.8
  371.7 76.8 %fold_backward.1 = (bf16[4,256,2048]{2,1,0:T(8,128)(2,1)S(1)}, f32[256,2048]{1,0:T(8,128)S(1)}, f32[1,2048]{1,0:T(1,128)S(1)}) custom-call(bf16[4,256,2048]{2,1,0:T(8,128)(2,1)S(1)} %bitcast.206, bf16[256,2048]{1,0:T(8,128)(2,1)} %bitcast.18.refs_1_, f32[256,2048]{1,0:T(8,128)S(1)} %copy-done.4, f32[1,2048]{1,0:T(1,128)S(1)} %reshape.401.refs_2_.refs_3_), custom_call_target="tpu_custom_call" | custom-call | tf_op jit(solution)/shard_map/fold_backward/pallas_call | solution.py:521
  450.9 5.7 multiply_reduce_fusion
  456.6 3.1 subtract_convert_fusion.grad_output
  459.7 2.4 collective-permute-done.20
  463.6 2.4 convolution_convert_fusion.6
  469.6 1.7 collective-permute-start.23
  473.1 2.2 copy-done.1
  476.9 21.2 %mixer_backward.1 = (bf16[1024,1536]{1,0:T(8,128)(2,1)S(1)}, f32[64,1024]{1,0:T(8,128)S(1)}) custom-call(s32[1]{0:T(128)} %bitcast.mine, bf16[1024,2048]{1,0:T(8,128)(2,1)S(1)} %copy-done.1, bf16[1024,2048]{1,0:T(8,128)(2,1)S(1)} %copy-done.1, bf16[1024,2048]{1,0:T(8,128)(2,1)S(1)} %copy-done.1, bf16[1024,512]{1,0:T(8,128)(2,1)S(1)} %copy-done.11, ...), custom_call_target="tpu_custom_call" | custom-call | flops 2097152000 | bytes 10485760 | tf_op jit(solution)/shard_map/mixer_backward/pallas_call | solution.py:310
  499.8 11.6 %convolution_convert_fusion = bf16[2048,2048]{1,0:T(8,128)(2,1)} fusion(bf16[1024,2048]{1,0:T(8,128)(2,1)S(1)} %copy-done.20, bf16[1024,512]{1,0:T(8,128)(2,1)S(1)} %copy-done.34, bf16[1024,1536]{1,0:T(8,128)(2,1)S(1)} %get-tuple-element.82), kind=kOutput, calls=%fused_computation.8 | convolution fusion | flops 8602517504 | bytes 16777216 | tf_op jit(solution)/shard_map/dot_general | solution.py:33
  515.2 2.6 pad_maximum_fusion.1
  519.4 11.4 %fusion.46 = f32[1024,2048]{1,0:T(8,128)S(1)} fusion(bf16[1024,2048]{1,0:T(8,128)(2,1)S(1)} %pad_maximum_fusion.1, bf16[2048,2048]{1,0:T(8,128)(2,1)} %all-gather.7.cloned.1.call-done), kind=kOutput, calls=%fused_computation.254 | convolution fusion | flops 8589934592 | bytes 20971520 | tf_op jit(solution)/shard_map/dot_general | solution.py:29
  530.9 1.9 fusion.3
  546.1 2.7 collective-permute-done.29
  548.7 6.7 %collective-permute-done.28 = bf16[64,2816]{1,0:T(8,128)(2,1)} collective-permute-done((bf16[64,2816]{1,0:T(8,128)(2,1)}, bf16[64,2816]{1,0:T(8,128)(2,1)}, u32[]{:S(2)}, u32[]{:S(2)}) %collective-permute-start.28) | collective-permute-done | bytes 360480 | tf_op jit(solution)/shard_map/ppermute | solution.py:542
  557.2 8.5 %collective-permute-done.25 = bf16[128,2048]{1,0:T(8,128)(2,1)} collective-permute-done((bf16[128,2048]{1,0:T(8,128)(2,1)}, bf16[128,2048]{1,0:T(8,128)(2,1)}, u32[]{:S(2)}, u32[]{:S(2)}) %collective-permute-start.25) | collective-permute-done | bytes 524320 | tf_op jit(solution)/shard_map/ppermute | solution.py:542
  566.6 2.0 add_convert_fusion.3
  570.9 3.5 fusion.17
  576.7 17.0 %collective-permute-done.30 = bf16[256,2048]{1,0:T(8,128)(2,1)S(1)} collective-permute-done((bf16[256,2048]{1,0:T(8,128)(2,1)S(1)}, bf16[256,2048]{1,0:T(8,128)(2,1)S(1)}, u32[]{:S(2)}, u32[]{:S(2)}) %collective-permute-start.30) | collective-permute-done | bytes 1048608 | tf_op jit(solution)/shard_map/ppermute | solution.py:542
  598.6 1.7 collective-permute-start.32
  600.3 3.2 maximum_convert_fusion
  604.8 3.3 convert_add_fusion
  608.1 1.9 copy.70
  610.1 2.5 collective-permute-start.34
  618.0 3.0 copy.72
  621.2 3.2 fusion.18
  626.4 1.7 collective-permute-start.39
  632.9 3.6 collective-permute-done.39
  636.5 5.1 collective-permute-done.38
  (377 shorter events, 115.4 us)
Async XLA Ops:
  7.2 108.7 %all-gather.5.cloned.1.call-start = ((), (), s32[]{:S(2)}) async-start(), calls=%async_computation.4 | async-start | bytes 2359296 | tf_op jit(solution)/shard_map/all_gather | solution.py:734
  7.9 118.0 %all-gather.7.cloned.1.call-start = ((), (), s32[]{:S(2)}) async-start(), calls=%async_computation.5 | async-start | bytes 9437184 | tf_op jit(solution)/shard_map/all_gather | solution.py:738
  15.4 11.1 %collective-permute-start.11 = (bf16[64,2048]{1,0:T(8,128)(2,1)S(1)}, bf16[64,2048]{1,0:T(8,128)(2,1)S(1)}, u32[]{:S(2)}, u32[]{:S(2)}) collective-permute-start(bf16[64,2048]{1,0:T(8,128)(2,1)S(1)} %bitcast.235), channel_id=1, source_target_pairs={{0,24},{8,16},{16,8},{24,0},{1,25},{9,17},{17,9},{25,1},{2,26},{10... | collective-permute-start | bytes 786440 | tf_op jit(solution)/shard_map/ppermute | solution.py:542
  19.5 11.8 %collective-permute-start.10 = (bf16[64,2048]{1,0:T(8,128)(2,1)S(1)}, bf16[64,2048]{1,0:T(8,128)(2,1)S(1)}, u32[]{:S(2)}, u32[]{:S(2)}) collective-permute-start(bf16[64,2048]{1,0:T(8,128)(2,1)S(1)} %bitcast.236), channel_id=1, source_target_pairs={{0,16},{8,24},{16,0},{24,8},{1,17},{9,25},{17,1},{25,9},{2,18},{10... | collective-permute-start | bytes 786440 | tf_op jit(solution)/shard_map/ppermute | solution.py:542
  20.2 11.3 %collective-permute-start.9 = (bf16[64,2048]{1,0:T(8,128)(2,1)S(1)}, bf16[64,2048]{1,0:T(8,128)(2,1)S(1)}, u32[]{:S(2)}, u32[]{:S(2)}) collective-permute-start(bf16[64,2048]{1,0:T(8,128)(2,1)S(1)} %bitcast.237), channel_id=1, source_target_pairs={{0,8},{8,0},{16,24},{24,16},{1,9},{9,1},{17,25},{25,17},{2,10},{10... | collective-permute-start | bytes 786440 | tf_op jit(solution)/shard_map/ppermute | solution.py:542
  33.0 234.0 %all-gather.9.cloned.1.call-start = ((), (), s32[]{:S(2)}) async-start(), calls=%async_computation.6 | async-start | bytes 12976128 | tf_op jit(solution)/shard_map/all_gather | solution.py:740
  37.2 12.3 %collective-permute-start.18 = (bf16[64,2816]{1,0:T(8,128)(2,1)S(1)}, bf16[64,2816]{1,0:T(8,128)(2,1)S(1)}, u32[]{:S(2)}, u32[]{:S(2)}) collective-permute-start(bf16[64,2816]{1,0:T(8,128)(2,1)S(1)} %bitcast.227), channel_id=1, source_target_pairs={{0,24},{8,16},{16,8},{24,0},{1,25},{9,17},{17,9},{25,1},{2,26},{10... | collective-permute-start | bytes 1081352 | tf_op jit(solution)/shard_map/ppermute | solution.py:542
  39.1 17.0 %collective-permute-start.17 = (bf16[64,2816]{1,0:T(8,128)(2,1)S(1)}, bf16[64,2816]{1,0:T(8,128)(2,1)S(1)}, u32[]{:S(2)}, u32[]{:S(2)}) collective-permute-start(bf16[64,2816]{1,0:T(8,128)(2,1)S(1)} %bitcast.228), channel_id=1, source_target_pairs={{0,16},{8,24},{16,0},{24,8},{1,17},{9,25},{17,1},{25,9},{2,18},{10... | collective-permute-start | bytes 1081352 | tf_op jit(solution)/shard_map/ppermute | solution.py:542
  40.4 16.0 %collective-permute-start.16 = (bf16[64,2816]{1,0:T(8,128)(2,1)S(1)}, bf16[64,2816]{1,0:T(8,128)(2,1)S(1)}, u32[]{:S(2)}, u32[]{:S(2)}) collective-permute-start(bf16[64,2816]{1,0:T(8,128)(2,1)S(1)} %bitcast.229), channel_id=1, source_target_pairs={{0,8},{8,0},{16,24},{24,16},{1,9},{9,1},{17,25},{25,17},{2,10},{10... | collective-permute-start | bytes 1081352 | tf_op jit(solution)/shard_map/ppermute | solution.py:542
  56.8 16.0 %copy-start.2 = (bf16[1,256,2048]{2,1,0:T(8,128)(2,1)S(1)}, bf16[1,256,2048]{2,1,0:T(8,128)(2,1)}, u32[]{:S(2)}) copy-start(bf16[1,256,2048]{2,1,0:T(8,128)(2,1)} %param.17) | copy-start | bytes 3145732
  58.1 241.4 %all-gather.11.cloned.1.call-start = ((), (), s32[]{:S(2)}) async-start(), calls=%async_computation.7 | async-start | bytes 6488064 | tf_op jit(solution)/shard_map/all_gather | solution.py:741
  58.9 1.2 collective-permute-start.4
  60.1 3.8 collective-permute-start.5
  64.0 7.1 %collective-permute-start.6 = (bf16[4,1608]{1,0:T(4,128)(2,1)S(1)}, bf16[4,1608]{1,0:T(4,128)(2,1)S(1)}, u32[]{:S(2)}, u32[]{:S(2)}) collective-permute-start(bf16[4,1608]{1,0:T(4,128)(2,1)S(1)} %pad_maximum_fusion.28), channel_id=1, source_target_pairs={{0,4},{1,5},{2,6},{3,7},{4,0},{5,1},{6,2},{7,3},{8,12},{9,13},{10,... | collective-permute-start | bytes 38600 | tf_op jit(solution)/shard_map/ppermute | solution.py:580
  71.2 6.8 %collective-permute-start.7 = (bf16[8,1608]{1,0:T(8,128)(2,1)S(1)}, bf16[8,1608]{1,0:T(8,128)(2,1)S(1)}, u32[]{:S(2)}, u32[]{:S(2)}) collective-permute-start(bf16[8,1608]{1,0:T(8,128)(2,1)S(1)} %pad_maximum_fusion.27), channel_id=1, source_target_pairs={{0,8},{8,0},{16,24},{24,16},{1,9},{9,1},{17,25},{25,17},{2,10},{10... | collective-permute-start | bytes 77192 | tf_op jit(solution)/shard_map/ppermute | solution.py:580
  75.9 28.9 %collective-permute-start = (bf16[256,2048]{1,0:T(8,128)(2,1)S(1)}, bf16[256,2048]{1,0:T(8,128)(2,1)}, u32[]{:S(2)}, u32[]{:S(2)}) collective-permute-start(bf16[256,2048]{1,0:T(8,128)(2,1)S(1)} %copy.61), channel_id=1, source_target_pairs={{0,8},{8,0},{16,24},{24,16},{1,9},{9,1},{17,25},{25,17},{2,10},{10... | collective-permute-start | bytes 3145736 | tf_op jit(solution)/shard_map/ppermute | solution.py:542
  76.5 23.7 %collective-permute-start.1 = (bf16[256,2048]{1,0:T(8,128)(2,1)S(1)}, bf16[256,2048]{1,0:T(8,128)(2,1)}, u32[]{:S(2)}, u32[]{:S(2)}) collective-permute-start(bf16[256,2048]{1,0:T(8,128)(2,1)S(1)} %copy.61), channel_id=1, source_target_pairs={{0,16},{8,24},{16,0},{24,8},{1,17},{9,25},{17,1},{25,9},{2,18},{10... | collective-permute-start | bytes 3145736 | tf_op jit(solution)/shard_map/ppermute | solution.py:542
  78.0 20.7 %collective-permute-start.8 = (bf16[16,1608]{1,0:T(8,128)(2,1)S(1)}, bf16[16,1608]{1,0:T(8,128)(2,1)S(1)}, u32[]{:S(2)}, u32[]{:S(2)}) collective-permute-start(bf16[16,1608]{1,0:T(8,128)(2,1)S(1)} %pad_maximum_fusion.26), channel_id=1, source_target_pairs={{0,16},{8,24},{16,0},{24,8},{1,17},{9,25},{17,1},{25,9},{2,18},{10... | collective-permute-start | bytes 154376 | tf_op jit(solution)/shard_map/ppermute | solution.py:580
  102.1 9.5 %collective-permute-start.2 = (bf16[128,2048]{1,0:T(8,128)(2,1)}, bf16[128,2048]{1,0:T(8,128)(2,1)}, u32[]{:S(2)}, u32[]{:S(2)}) collective-permute-start(bf16[128,2048]{1,0:T(8,128)(2,1)} %slice.292), channel_id=1, source_target_pairs={{0,8},{8,0},{16,24},{24,16},{1,9},{9,1},{17,25},{25,17},{2,10},{10... | collective-permute-start | bytes 1572872 | tf_op jit(solution)/shard_map/ppermute | solution.py:542
  104.4 16.4 %copy-start.39 = (bf16[16,2048]{1,0:T(8,128)(2,1)}, bf16[16,2048]{1,0:T(8,128)(2,1)S(1)}, u32[]{:S(2)}) copy-start(bf16[16,2048]{1,0:T(8,128)(2,1)S(1)} %reshape.368) | copy-start | bytes 196612
  104.5 19.4 %copy-start.49 = (bf16[256,16]{1,0:T(8,128)(2,1)}, bf16[256,16]{1,0:T(8,128)(2,1)S(1)}, u32[]{:S(2)}) copy-start(bf16[256,16]{1,0:T(8,128)(2,1)S(1)} %reshape.365) | copy-start | bytes 24580
  104.7 263.0 %reduce-scatter.5.cloned.1.call-start = ((), (), s32[]{:S(2)}) async-start(), calls=%async_computation.8 | async-start | bytes 6488064 | tf_op jit(solution)/shard_map/reduce_scatter | solution.py:833
  105.9 9.2 %collective-permute-start.3 = (bf16[128,2048]{1,0:T(8,128)(2,1)S(1)}, bf16[128,2048]{1,0:T(8,128)(2,1)S(1)}, u32[]{:S(2)}, u32[]{:S(2)}) collective-permute-start(bf16[128,2048]{1,0:T(8,128)(2,1)S(1)} %slice.293), channel_id=1, source_target_pairs={{0,16},{8,24},{16,0},{24,8},{1,17},{9,25},{17,1},{25,9},{2,18},{10... | collective-permute-start | bytes 1572872 | tf_op jit(solution)/shard_map/ppermute | solution.py:542
  124.0 17.2 %copy-start.47 = (bf16[1024,16]{0,1:T(8,128)(2,1)}, bf16[1024,16]{0,1:T(8,128)(2,1)S(1)}, u32[]{:S(2)}) copy-start(bf16[1024,16]{0,1:T(8,128)(2,1)S(1)} %convolution_convert_fusion.8) | copy-start | bytes 98308
  125.9 15.4 %copy-start.6 = (f32[128,1024]{1,0:T(8,128)S(1)}, f32[128,1024]{1,0:T(8,128)}, u32[]{:S(2)}) copy-start(f32[128,1024]{1,0:T(8,128)} %pad_maximum_fusion.22.rate) | copy-start | bytes 1572868
  125.9 34.3 %collective-permute-start.12 = (bf16[256,2048]{1,0:T(8,128)(2,1)}, bf16[256,2048]{1,0:T(8,128)(2,1)S(1)}, u32[]{:S(2)}, u32[]{:S(2)}) collective-permute-start(bf16[256,2048]{1,0:T(8,128)(2,1)} %bitcast.18.refs_1_), channel_id=1, source_target_pairs={{0,8},{8,0},{16,24},{24,16},{1,9},{9,1},{17,25},{25,17},{2,10},{10... | collective-permute-start | bytes 3145736 | tf_op jit(solution)/shard_map/ppermute | solution.py:542
  127.3 30.8 %collective-permute-start.13 = (bf16[256,2048]{1,0:T(8,128)(2,1)}, bf16[256,2048]{1,0:T(8,128)(2,1)S(1)}, u32[]{:S(2)}, u32[]{:S(2)}) collective-permute-start(bf16[256,2048]{1,0:T(8,128)(2,1)} %bitcast.18.refs_1_), channel_id=1, source_target_pairs={{0,16},{8,24},{16,0},{24,8},{1,17},{9,25},{17,1},{25,9},{2,18},{10... | collective-permute-start | bytes 3145736 | tf_op jit(solution)/shard_map/ppermute | solution.py:542
  141.2 12.0 %copy-start = (bf16[1024,2048]{1,0:T(8,128)(2,1)}, bf16[1024,2048]{1,0:T(8,128)(2,1)S(1)}, u32[]{:S(2)}) copy-start(bf16[1024,2048]{1,0:T(8,128)(2,1)S(1)} %get-tuple-element.247.query.key.value) | copy-start | bytes 12582916
  141.2 12.2 %copy-start.30 = (f32[1024,2048]{1,0:T(8,128)}, f32[1024,2048]{1,0:T(8,128)S(1)}, u32[]{:S(2)}) copy-start(f32[1024,2048]{1,0:T(8,128)S(1)} %get-tuple-element.248) | copy-start | bytes 25165828
  158.2 13.6 %collective-permute-start.14 = (bf16[128,2048]{1,0:T(8,128)(2,1)S(1)}, bf16[128,2048]{1,0:T(8,128)(2,1)S(1)}, u32[]{:S(2)}, u32[]{:S(2)}) collective-permute-start(bf16[128,2048]{1,0:T(8,128)(2,1)S(1)} %slice.296), channel_id=1, source_target_pairs={{0,8},{8,0},{16,24},{24,16},{1,9},{9,1},{17,25},{25,17},{2,10},{10... | collective-permute-start | bytes 1572872 | tf_op jit(solution)/shard_map/ppermute | solution.py:542
  160.2 13.3 %collective-permute-start.15 = (bf16[128,2048]{1,0:T(8,128)(2,1)S(1)}, bf16[128,2048]{1,0:T(8,128)(2,1)S(1)}, u32[]{:S(2)}, u32[]{:S(2)}) collective-permute-start(bf16[128,2048]{1,0:T(8,128)(2,1)S(1)} %slice.297), channel_id=1, source_target_pairs={{0,16},{8,24},{16,0},{24,8},{1,17},{9,25},{17,1},{25,9},{2,18},{10... | collective-permute-start | bytes 1572872 | tf_op jit(solution)/shard_map/ppermute | solution.py:542
  299.4 173.4 %reduce-scatter.7.cloned.1.call-start = ((), (), s32[]{:S(2)}) async-start(), calls=%async_computation.9 | async-start | bytes 7208960 | tf_op jit(solution)/shard_map/reduce_scatter | solution.py:633
  316.4 17.8 %copy-start.10 = (bf16[4,256,2048]{2,1,0:T(8,128)(2,1)S(1)}, bf16[4,256,2048]{2,1,0:T(8,128)(2,1)}, u32[]{:S(2)}) copy-start(bf16[4,256,2048]{2,1,0:T(8,128)(2,1)} %copy-done.9) | copy-start | bytes 12582916
  346.1 12.9 %collective-permute-start.19 = (bf16[1024,2816]{1,0:T(8,128)(2,1)}, bf16[1024,2816]{1,0:T(8,128)(2,1)S(1)}, u32[]{:S(2)}, u32[]{:S(2)}) collective-permute-start(bf16[1024,2816]{1,0:T(8,128)(2,1)} %convolution_convert_fusion.2), channel_id=1, source_target_pairs={{0,1},{1,0},{2,3},{3,2},{4,5},{5,4},{6,7},{7,6},{8,9},{9,8},{10,11... | collective-permute-start | bytes 17301512 | tf_op jit(solution)/shard_map/ppermute | solution.py:580
  348.0 11.1 %copy-start.67 = (bf16[1024,1408]{1,0:T(8,128)(2,1)S(1)}, bf16[1024,1408]{1,0:T(8,128)(2,1)}, u32[]{:S(2)}) copy-start(bf16[1024,1408]{1,0:T(8,128)(2,1)} %get-tuple-element.135) | copy-start | bytes 8650756
  367.7 143.7 %reduce-scatter.9.cloned.1.call-start = ((), (), s32[]{:S(2)}) async-start(), calls=%async_computation.10 | async-start | bytes 1310720 | tf_op jit(solution)/shard_map/reduce_scatter | solution.py:633
  371.7 76.8 %copy-start.27 = (bf16[1024,2048]{1,0:T(8,128)(2,1)S(1)}, bf16[1024,2048]{1,0:T(8,128)(2,1)}, u32[]{:S(2)}) copy-start(bf16[1024,2048]{1,0:T(8,128)(2,1)} %convolution_convert_fusion.4) | copy-start | bytes 12582916
  448.8 13.4 %collective-permute-start.20 = (bf16[128,2048]{1,0:T(8,128)(2,1)S(1)}, bf16[128,2048]{1,0:T(8,128)(2,1)S(1)}, u32[]{:S(2)}, u32[]{:S(2)}) collective-permute-start(bf16[128,2048]{1,0:T(8,128)(2,1)S(1)} %get-tuple-element.149), channel_id=1, source_target_pairs={{0,8},{8,0},{16,24},{24,16},{1,9},{9,1},{17,25},{25,17},{2,10},{10... | collective-permute-start | bytes 1572872 | tf_op jit(solution)/shard_map/ppermute | solution.py:542
  450.3 13.3 %collective-permute-start.21 = (bf16[128,2048]{1,0:T(8,128)(2,1)S(1)}, bf16[128,2048]{1,0:T(8,128)(2,1)S(1)}, u32[]{:S(2)}, u32[]{:S(2)}) collective-permute-start(bf16[128,2048]{1,0:T(8,128)(2,1)S(1)} %get-tuple-element.148), channel_id=1, source_target_pairs={{0,16},{8,24},{16,0},{24,8},{1,17},{9,25},{17,1},{25,9},{2,18},{10... | collective-permute-start | bytes 1572872 | tf_op jit(solution)/shard_map/ppermute | solution.py:542
  466.6 4.7 collective-permute-start.24
  468.2 30.0 %collective-permute-start.22 = (bf16[256,2048]{1,0:T(8,128)(2,1)}, bf16[256,2048]{1,0:T(8,128)(2,1)}, u32[]{:S(2)}, u32[]{:S(2)}) collective-permute-start(bf16[256,2048]{1,0:T(8,128)(2,1)} %pad_maximum_fusion.15), channel_id=1, source_target_pairs={{0,8},{8,0},{16,24},{24,16},{1,9},{9,1},{17,25},{25,17},{2,10},{10... | collective-permute-start | bytes 3145736 | tf_op jit(solution)/shard_map/ppermute | solution.py:542
  469.6 28.5 %collective-permute-start.23 = (bf16[256,2048]{1,0:T(8,128)(2,1)}, bf16[256,2048]{1,0:T(8,128)(2,1)}, u32[]{:S(2)}, u32[]{:S(2)}) collective-permute-start(bf16[256,2048]{1,0:T(8,128)(2,1)} %pad_maximum_fusion.16), channel_id=1, source_target_pairs={{0,16},{8,24},{16,0},{24,8},{1,17},{9,25},{17,1},{25,9},{2,18},{10... | collective-permute-start | bytes 3145736 | tf_op jit(solution)/shard_map/ppermute | solution.py:542
  472.8 152.3 %reduce-scatter.11.cloned.1.call-start = ((), (), s32[]{:S(2)}) async-start(), calls=%async_computation.11 | async-start | bytes 9437184 | tf_op jit(solution)/shard_map/reduce_scatter | solution.py:889
  476.9 22.9 %copy-start.20 = (bf16[1024,2048]{1,0:T(8,128)(2,1)S(1)}, bf16[1024,2048]{1,0:T(8,128)(2,1)}, u32[]{:S(2)}) copy-start(bf16[1024,2048]{1,0:T(8,128)(2,1)} %copy-done.19) | copy-start | bytes 12582916
  476.9 22.9 %copy-start.34 = (bf16[1024,512]{1,0:T(8,128)(2,1)S(1)}, bf16[1024,512]{1,0:T(8,128)(2,1)}, u32[]{:S(2)}) copy-start(bf16[1024,512]{1,0:T(8,128)(2,1)} %get-tuple-element.136) | copy-start | bytes 3145732
  519.4 11.5 %copy-start.23 = (bf16[1024,2048]{1,0:T(8,128)(2,1)S(1)}, bf16[1024,2048]{1,0:T(8,128)(2,1)}, u32[]{:S(2)}) copy-start(bf16[1024,2048]{1,0:T(8,128)(2,1)} %constant_dynamic-update-slice_fusion) | copy-start | bytes 12582916
  519.4 11.5 %copy-start.40 = (bf16[16,2048]{1,0:T(8,128)(2,1)S(1)}, bf16[16,2048]{1,0:T(8,128)(2,1)}, u32[]{:S(2)}) copy-start(bf16[16,2048]{1,0:T(8,128)(2,1)} %copy-done.39) | copy-start | bytes 196612
  519.4 11.5 %copy-start.51 = (f32[1024]{0:T(1024)S(1)}, f32[1024]{0:T(1024)}, u32[]{:S(2)}) copy-start(f32[1024]{0:T(1024)} %copy-done.50) | copy-start | bytes 12292
  536.2 12.6 %collective-permute-start.29 = (bf16[64,2816]{1,0:T(8,128)(2,1)}, bf16[64,2816]{1,0:T(8,128)(2,1)}, u32[]{:S(2)}, u32[]{:S(2)}) collective-permute-start(bf16[64,2816]{1,0:T(8,128)(2,1)} %get-tuple-element.180), channel_id=1, source_target_pairs={{0,24},{8,16},{16,8},{24,0},{1,25},{9,17},{17,9},{25,1},{2,26},{10... | collective-permute-start | bytes 1081352 | tf_op jit(solution)/shard_map/ppermute | solution.py:542
  537.7 17.8 %collective-permute-start.28 = (bf16[64,2816]{1,0:T(8,128)(2,1)}, bf16[64,2816]{1,0:T(8,128)(2,1)}, u32[]{:S(2)}, u32[]{:S(2)}) collective-permute-start(bf16[64,2816]{1,0:T(8,128)(2,1)} %get-tuple-element.181), channel_id=1, source_target_pairs={{0,16},{8,24},{16,0},{24,8},{1,17},{9,25},{17,1},{25,9},{2,18},{10... | collective-permute-start | bytes 1081352 | tf_op jit(solution)/shard_map/ppermute | solution.py:542
  538.1 17.4 %collective-permute-start.27 = (bf16[64,2816]{1,0:T(8,128)(2,1)S(1)}, bf16[64,2816]{1,0:T(8,128)(2,1)}, u32[]{:S(2)}, u32[]{:S(2)}) collective-permute-start(bf16[64,2816]{1,0:T(8,128)(2,1)S(1)} %get-tuple-element.182), channel_id=1, source_target_pairs={{0,8},{8,0},{16,24},{24,16},{1,9},{9,1},{17,25},{25,17},{2,10},{10... | collective-permute-start | bytes 1081352 | tf_op jit(solution)/shard_map/ppermute | solution.py:542
  540.3 25.3 %collective-permute-start.25 = (bf16[128,2048]{1,0:T(8,128)(2,1)}, bf16[128,2048]{1,0:T(8,128)(2,1)}, u32[]{:S(2)}, u32[]{:S(2)}) collective-permute-start(bf16[128,2048]{1,0:T(8,128)(2,1)} %get-tuple-element.143), channel_id=1, source_target_pairs={{0,8},{8,0},{16,24},{24,16},{1,9},{9,1},{17,25},{25,17},{2,10},{10... | collective-permute-start | bytes 1572872 | tf_op jit(solution)/shard_map/ppermute | solution.py:542
  540.8 25.8 %collective-permute-start.26 = (bf16[128,2048]{1,0:T(8,128)(2,1)}, bf16[128,2048]{1,0:T(8,128)(2,1)}, u32[]{:S(2)}, u32[]{:S(2)}) collective-permute-start(bf16[128,2048]{1,0:T(8,128)(2,1)} %get-tuple-element.142), channel_id=1, source_target_pairs={{0,16},{8,24},{16,0},{24,8},{1,17},{9,25},{17,1},{25,9},{2,18},{10... | collective-permute-start | bytes 1572872 | tf_op jit(solution)/shard_map/ppermute | solution.py:542
  568.7 25.1 %collective-permute-start.30 = (bf16[256,2048]{1,0:T(8,128)(2,1)S(1)}, bf16[256,2048]{1,0:T(8,128)(2,1)S(1)}, u32[]{:S(2)}, u32[]{:S(2)}) collective-permute-start(bf16[256,2048]{1,0:T(8,128)(2,1)S(1)} %pad_maximum_fusion.19), channel_id=1, source_target_pairs={{0,8},{8,0},{16,24},{24,16},{1,9},{9,1},{17,25},{25,17},{2,10},{10... | collective-permute-start | bytes 3145736 | tf_op jit(solution)/shard_map/ppermute | solution.py:542
  569.5 24.8 %collective-permute-start.31 = (bf16[256,2048]{1,0:T(8,128)(2,1)S(1)}, bf16[256,2048]{1,0:T(8,128)(2,1)}, u32[]{:S(2)}, u32[]{:S(2)}) collective-permute-start(bf16[256,2048]{1,0:T(8,128)(2,1)S(1)} %pad_maximum_fusion.20), channel_id=1, source_target_pairs={{0,16},{8,24},{16,0},{24,8},{1,17},{9,25},{17,1},{25,9},{2,18},{10... | collective-permute-start | bytes 3145736 | tf_op jit(solution)/shard_map/ppermute | solution.py:542
  574.5 19.8 %copy-start.53 = (f32[2048]{0:T(1024)S(1)}, f32[2048]{0:T(1024)}, u32[]{:S(2)}) copy-start(f32[2048]{0:T(1024)} %reshape.384) | copy-start | bytes 24580
  598.6 4.9 collective-permute-start.32
  603.5 6.5 %collective-permute-start.33 = (f32[8,1352]{1,0:T(8,128)S(1)}, f32[8,1352]{1,0:T(8,128)S(1)}, u32[]{:S(2)}, u32[]{:S(2)}) collective-permute-start(f32[8,1352]{1,0:T(8,128)S(1)} %slice_select_fusion.1), channel_id=1, source_target_pairs={{0,8},{8,0},{16,24},{24,16},{1,9},{9,1},{17,25},{25,17},{2,10},{10... | collective-permute-start | bytes 129800 | tf_op jit(solution)/shard_map/ppermute | solution.py:580
  610.1 4.8 collective-permute-start.34
  614.9 6.1 collective-permute-start.35
  621.1 3.4 collective-permute-start.36
  626.4 10.1 %collective-permute-start.39 = (bf16[64,2048]{1,0:T(8,128)(2,1)S(1)}, bf16[64,2048]{1,0:T(8,128)(2,1)S(1)}, u32[]{:S(2)}, u32[]{:S(2)}) collective-permute-start(bf16[64,2048]{1,0:T(8,128)(2,1)S(1)} %get-tuple-element.208), channel_id=1, source_target_pairs={{0,24},{8,16},{16,8},{24,0},{1,25},{9,17},{17,9},{25,1},{2,26},{10... | collective-permute-start | bytes 786440 | tf_op jit(solution)/shard_map/ppermute | solution.py:542
  628.1 13.5 %collective-permute-start.38 = (bf16[64,2048]{1,0:T(8,128)(2,1)S(1)}, bf16[64,2048]{1,0:T(8,128)(2,1)S(1)}, u32[]{:S(2)}, u32[]{:S(2)}) collective-permute-start(bf16[64,2048]{1,0:T(8,128)(2,1)S(1)} %get-tuple-element.209), channel_id=1, source_target_pairs={{0,16},{8,24},{16,0},{24,8},{1,17},{9,25},{17,1},{25,9},{2,18},{10... | collective-permute-start | bytes 786440 | tf_op jit(solution)/shard_map/ppermute | solution.py:542
  628.7 13.0 %collective-permute-start.37 = (bf16[64,2048]{1,0:T(8,128)(2,1)S(1)}, bf16[64,2048]{1,0:T(8,128)(2,1)S(1)}, u32[]{:S(2)}, u32[]{:S(2)}) collective-permute-start(bf16[64,2048]{1,0:T(8,128)(2,1)S(1)} %get-tuple-element.210), channel_id=1, source_target_pairs={{0,8},{8,0},{16,24},{24,16},{1,9},{9,1},{17,25},{25,17},{2,10},{10... | collective-permute-start | bytes 786440 | tf_op jit(solution)/shard_map/ppermute | solution.py:542
  (52 other events, 170.8 us)
Sparse Core Ops, SparseCore 0:
  9.6 31.7 all-gather.4
  43.6 82.1 all-gather.6
  128.0 106.4 all-gather.8
  236.0 58.7 all-gather.10
  299.5 64.9 reduce-scatter.4
  367.8 102.3 reduce-scatter.6
  473.0 27.6 reduce-scatter.8
  511.5 89.6 reduce-scatter.10

commit v14 on v13

--- a/solution.py
+++ b/solution.py
@@ -894,8 +894,8 @@
     term_mixer = restored(jnp.sum(grad_normed * plain_one, axis=0))
     term_squeeze = restored(dot_tn(grad_reduced, normed))
     feed_share = exchanged(after(feed_sum, term_pre).reshape(ring, own, 2 * hidden_part), mine, ring)
-    grad_normed, feed_share, (term_mixer, term_squeeze) = scattered(
-        grad_normed.astype(BF16), ring, feed_share, (term_mixer, term_squeeze)
+    grad_normed, (feed_share, term_mixer, term_squeeze), _ = scattered(
+        grad_normed.astype(BF16), ring, (feed_share, term_mixer, term_squeeze), term_bias
     )
     grad_normed = restored(grad_normed)
     inputs_own = input_own.astype(F32)

time: 660 us -> 655 us (level)
  waiting for transfers between devices: 118 us -> 109 us
    ppermute x28, waiting for transfers between devices: 89.7 us -> 72.3 us  [swapped(): return lax.ppermute(block, 'seq', [(i, i ^ by) for i in range(ring)])]
    ppermute x12, waiting for transfers between devices: 27.8 us -> 35.6 us  [flipped(): lax.ppermute(block, axis, [(i, i ^ by) for i in range(lax.axis_size(axis))])]
    unnamed x162 -> x168, local copies, waits for them, and re-layouts: 40.4 us -> 41.7 us
  transfers between devices with their start and end apart: 48 -> 48, of which waited for: 25 -> 26; matrix products, arithmetic and copies ran while one was open for 37% -> 38% of each run, Pallas kernels for 30% -> 31%
where the time goes in v14:
time: 655 us; the launch traced here: 647 us
  Pallas kernels  198 us (30%)
  matrix products  145 us (22%)
  waiting for transfers between devices  109 us (17%)
  local copies, waits for them, and re-layouts  88.9 us (14%)
  other arithmetic  46.3 us (7%)
  starting transfers between devices  43.6 us (7%)
  between operations  16.1 us (2%)
    pallas_call x2, Pallas kernels, fold(): pl.pallas_call(functools.partial(fold_kernel, finish, len(given)), out_sh...  165 us
    ppermute x28, waiting for transfers between devices, swapped(): return lax.ppermute(block, 'seq', [(i, i ^ by) for i in range(ring)])  72.3 us
    dot_general x6, matrix products, dot_nt(): lax.dot_general(left, right, (((1,), (1,)), ((), ())), preferred_element_...  52.5 us
    dot_general x7, matrix products, dot_tn(): lax.dot_general(left, right, (((0,), (0,)), ((), ())), preferred_element_...  46.6 us
    dot_general x6, matrix products, dot_nn(): lax.dot_general(left, right, (((1,), (0,)), ((), ())), preferred_element_...  46 us
    unnamed x168, local copies, waits for them, and re-layouts  41.7 us
    ppermute x12, waiting for transfers between devices, flipped(): lax.ppermute(block, axis, [(i, i ^ by) for i in range(lax.axis_size(axis))])  35.6 us
    ppermute x28, starting transfers between devices, swapped(): return lax.ppermute(block, 'seq', [(i, i ^ by) for i in range(ring)])  31.2 us
  transfers between devices with their start and end apart: 48, of which 26 were waited for; matrix products, arithmetic and copies ran while one was open for 38% of the time, Pallas kernels for 31%

profile of v14, /device:TPU:0, one launch (start us, length us, event | category | flops | bytes accessed | tf_op | source)
XLA Modules:
  0.0 646.6 jit_solution(13035628546549975649)
XLA Ops:
  13.1 2.2 constant_dynamic-slice_fusion.22
  15.4 4.0 collective-permute-start.11
  20.5 6.0 collective-permute-done.11
  26.5 4.7 collective-permute-done.10
  34.2 3.0 constant_dynamic-slice_fusion.13
  41.0 8.5 %collective-permute-done.18 = bf16[64,2816]{1,0:T(8,128)(2,1)S(1)} collective-permute-done((bf16[64,2816]{1,0:T(8,128)(2,1)S(1)}, bf16[64,2816]{1,0:T(8,128)(2,1)S(1)}, u32[]{:S(2)}, u32[]{:S(2)}) %collective-permute-start.18) | collective-permute-done | bytes 360480 | tf_op jit(solution)/shard_map/ppermute | solution.py:542
  49.5 6.5 %collective-permute-done.17 = bf16[64,2816]{1,0:T(8,128)(2,1)S(1)} collective-permute-done((bf16[64,2816]{1,0:T(8,128)(2,1)S(1)}, bf16[64,2816]{1,0:T(8,128)(2,1)S(1)}, u32[]{:S(2)}, u32[]{:S(2)}) %collective-permute-start.17) | collective-permute-done | bytes 360480 | tf_op jit(solution)/shard_map/ppermute | solution.py:542
  61.8 2.2 collective-permute-done.5
  64.0 2.5 collective-permute-start.6
  66.6 4.6 collective-permute-done.6
  79.7 19.1 %collective-permute-done.8 = bf16[16,1608]{1,0:T(8,128)(2,1)S(1)} collective-permute-done((bf16[16,1608]{1,0:T(8,128)(2,1)S(1)}, bf16[16,1608]{1,0:T(8,128)(2,1)S(1)}, u32[]{:S(2)}, u32[]{:S(2)}) %collective-permute-start.8) | collective-permute-done | bytes 51488 | tf_op jit(solution)/shard_map/ppermute | solution.py:580
  100.2 1.9 slice.292
  106.5 2.3 constant_dynamic-update-slice_fusion.3
  108.8 2.4 constant_dynamic-update-slice_fusion.2
  111.6 1.9 constant_dynamic-update-slice_fusion.1
  115.9 3.2 fusion.4
  120.8 2.0 copy-done.19
  128.7 12.5 %fusion.44 = (bf16[1024,2048]{1,0:T(8,128)(2,1)S(1)}, f32[1024,2048]{1,0:T(8,128)S(1)}) fusion(bf16[1024,2048]{1,0:T(8,128)(2,1)} %copy-done.19, bf16[2048,2048]{1,0:T(8,128)(2,1)} %all-gather.7.cloned.1.call-done), kind=kOutput, calls=%fused_computation.252 | convolution fusion | flops 8592031744 | bytes 25165824 | tf_op jit(solution)/shard_map/dot_general | solution.py:25
  141.3 11.9 %mixer_forward.1 = (f32[1024,512]{1,0:T(8,128)S(1)}, f32[128,1024]{1,0:T(8,128)S(1)}, f32[8,128,512]{2,1,0:T(8,128)S(1)}) custom-call(s32[1]{0:T(128)} %bitcast.mine, bf16[1024,2048]{1,0:T(8,128)(2,1)S(1)} %get-tuple-element.247.query.key.value, bf16[1024,2048]{1,0:T(8,128)(2,1)S(1)} %get-tuple-element.247.query.key.value, ...), custom_call_target="tpu_custom_call" | custom-call | flops 1048576000 | bytes 6291456 | tf_op jit(solution)/shard_map/mixer_forward/pallas_call | solution.py:285
  155.7 2.3 convolution_convert_fusion.5
  161.2 10.5 %collective-permute-done.14 = bf16[128,2048]{1,0:T(8,128)(2,1)S(1)} collective-permute-done((bf16[128,2048]{1,0:T(8,128)(2,1)S(1)}, bf16[128,2048]{1,0:T(8,128)(2,1)S(1)}, u32[]{:S(2)}, u32[]{:S(2)}) %collective-permute-start.14) | collective-permute-done | bytes 524320 | tf_op jit(solution)/shard_map/ppermute | solution.py:542
  173.6 2.0 copy-done.48
  175.6 87.9 %fold_forward.1 = (bf16[4,256,2048]{2,1,0:T(8,128)(2,1)S(1)}, f32[256,2048]{1,0:T(8,128)S(1)}) custom-call(bf16[4,256,2048]{2,1,0:T(8,128)(2,1)S(1)} %bitcast.205, bf16[256,2048]{1,0:T(8,128)(2,1)S(1)} %bitcast.204, f32[1,2048]{1,0:T(1,128)S(1)} %reshape.401.refs_2_.refs_3_), custom_call_target="tpu_custom_call" | custom-call | tf_op jit(solution)/shard_map/fold_forward/pallas_call | solution.py:521
  264.8 2.1 copy-done.9
  266.9 17.3 %fusion.45 = f32[1024,2816]{1,0:T(8,128)S(1)} fusion(bf16[1024,2048]{1,0:T(8,128)(2,1)} %bitcast.207, bf16[2048,2816]{1,0:T(8,128)(2,1)} %all-gather.9.cloned.1.call-done), kind=kOutput, calls=%fused_computation.253 | convolution fusion | flops 11811160064 | bytes 27262976 | tf_op jit(solution)/shard_map/dot_general | solution.py:25
  284.2 1.8 multiply_convert_fusion.2
  286.0 3.5 copy-done.25
  291.1 8.1 %convolution_convert_fusion.1 = bf16[1408,2048]{1,0:T(8,128)(2,1)} fusion(bf16[1024,1408]{1,0:T(8,128)(2,1)S(1)} %multiply_convert_fusion.2, bf16[1024,2048]{1,0:T(8,128)(2,1)S(1)} %copy-done.49), kind=kOutput, calls=%fused_computation.9 | convolution fusion | flops 5908463616 | bytes 12845056 | tf_op jit(solution)/shard_map/dot_general | solution.py:33
  299.3 15.4 %multiply_convert_fusion.1 = (bf16[1024,1408]{1,0:T(8,128)(2,1)S(1)}, bf16[1024,1408]{1,0:T(8,128)(2,1)}) fusion(f32[1024,2816]{1,0:T(8,128)} %copy-done.25, bf16[1024,2048]{1,0:T(8,128)(2,1)} %copy-done.48, bf16[1408,2048]{1,0:T(8,128)(2,1)} %all-gather.11.cloned.1.call-done), kind=kOutput, calls=%fused_computation.12 | convolution fusion | flops 5924323328 | bytes 27262976 | tf_op jit(solution)/shard_map/dot_general | solution.py:29
  316.3 17.8 %convolution_convert_fusion.3 = bf16[1024,2048]{1,0:T(8,128)(2,1)} fusion(bf16[2048,2816]{1,0:T(8,128)(2,1)} %all-gather.9.cloned.1.call-done, bf16[1024,1408]{1,0:T(8,128)(2,1)} %get-tuple-element.135, bf16[1024,1408]{1,0:T(8,128)(2,1)S(1)} %get-tuple-element.134), kind=kOutput, calls=%fused_computation.19 | convolution fusion | flops 11824791552 | bytes 21495808 | tf_op jit(solution)/shard_map/dot_general | solution.py:29
  334.4 11.5 %convolution_convert_fusion.2 = bf16[1024,2816]{1,0:T(8,128)(2,1)} fusion(pred[]{:T(512)S(6)} %eq.86, bf16[1024,1408]{1,0:T(8,128)(2,1)} %get-tuple-element.135, bf16[1024,1408]{1,0:T(8,128)(2,1)} %copy-done.68, bf16[1024,256]{1,0:T(8,128)(2,1)S(1)} %get-tuple-element.152, bf16[1024,256]{1,0:T(8,128)(2,1)S(1)} %get-tuple-element.153, ...), kind=kOutput, calls=%fused_computation.16 | convolution fusion | flops 5937823744 | bytes 15728641 | tf_op jit(solution)/shard_map/dot_general | solution.py:33
  347.8 11.1 %convolution_convert_fusion.4 = bf16[1024,2048]{1,0:T(8,128)(2,1)} fusion(bf16[1024,1408]{1,0:T(8,128)(2,1)S(1)} %copy-done.30, bf16[1408,2048]{1,0:T(8,128)(2,1)} %all-gather.11.cloned.1.call-done), kind=kOutput, calls=%fused_computation.20 | convolution fusion | flops 5907677184 | bytes 12845056 | tf_op jit(solution)/shard_map/dot_general | solution.py:25
  358.8 8.6 %add_convert_fusion = bf16[1024,2816]{1,0:T(8,128)(2,1)} fusion(bf16[1024,2816]{1,0:T(8,128)(2,1)S(1)} %collective-permute-done.19, bf16[1024,1024]{1,0:T(8,128)(2,1)S(1)} %broadcast_select_fusion, bf16[1024,1408]{1,0:T(8,128)(2,1)S(1)} %copy-done.70, bf16[1024,1408]{1,0:T(8,128)(2,1)S(1)} %copy-done.69), kind=kOutput, calls=%fused_computation | convolution fusion | flops 5925765120 | bytes 19398656 | tf_op jit(solution)/shard_map/dot_general | solution.py:33
  369.3 2.2 copy-done.8
  371.5 76.8 %fold_backward.1 = (bf16[4,256,2048]{2,1,0:T(8,128)(2,1)S(1)}, f32[256,2048]{1,0:T(8,128)S(1)}, f32[1,2048]{1,0:T(1,128)S(1)}) custom-call(bf16[4,256,2048]{2,1,0:T(8,128)(2,1)S(1)} %bitcast.206, bf16[256,2048]{1,0:T(8,128)(2,1)} %bitcast.18.refs_1_, f32[256,2048]{1,0:T(8,128)S(1)} %copy-done.4, f32[1,2048]{1,0:T(1,128)S(1)} %reshape.401.refs_2_.refs_3_), custom_call_target="tpu_custom_call" | custom-call | tf_op jit(solution)/shard_map/fold_backward/pallas_call | solution.py:521
  450.6 5.7 multiply_reduce_fusion
  456.4 3.1 subtract_convert_fusion.grad_output
  459.5 2.4 collective-permute-done.20
  463.4 2.4 convolution_convert_fusion.6
  472.9 2.2 copy-done.1
  476.7 21.2 %mixer_backward.1 = (bf16[1024,1536]{1,0:T(8,128)(2,1)S(1)}, f32[64,1024]{1,0:T(8,128)S(1)}) custom-call(s32[1]{0:T(128)} %bitcast.mine, bf16[1024,2048]{1,0:T(8,128)(2,1)S(1)} %copy-done.1, bf16[1024,2048]{1,0:T(8,128)(2,1)S(1)} %copy-done.1, bf16[1024,2048]{1,0:T(8,128)(2,1)S(1)} %copy-done.1, bf16[1024,512]{1,0:T(8,128)(2,1)S(1)} %copy-done.11, ...), custom_call_target="tpu_custom_call" | custom-call | flops 2097152000 | bytes 10485760 | tf_op jit(solution)/shard_map/mixer_backward/pallas_call | solution.py:310
  499.6 11.5 %convolution_convert_fusion = bf16[2048,2048]{1,0:T(8,128)(2,1)} fusion(bf16[1024,2048]{1,0:T(8,128)(2,1)S(1)} %copy-done.20, bf16[1024,512]{1,0:T(8,128)(2,1)S(1)} %copy-done.38, bf16[1024,1536]{1,0:T(8,128)(2,1)S(1)} %get-tuple-element.82), kind=kOutput, calls=%fused_computation.8 | convolution fusion | flops 8602517504 | bytes 16777216 | tf_op jit(solution)/shard_map/dot_general | solution.py:33
  515.5 2.8 pad_maximum_fusion.1
  519.9 11.4 %fusion.46 = f32[1024,2048]{1,0:T(8,128)S(1)} fusion(bf16[1024,2048]{1,0:T(8,128)(2,1)S(1)} %pad_maximum_fusion.1, bf16[2048,2048]{1,0:T(8,128)(2,1)} %all-gather.7.cloned.1.call-done), kind=kOutput, calls=%fused_computation.254 | convolution fusion | flops 8589934592 | bytes 20971520 | tf_op jit(solution)/shard_map/dot_general | solution.py:29
  531.4 1.9 fusion.3
  533.3 1.9 copy-done.24
  539.2 3.5 fusion.47
  554.7 3.5 fusion.17
  559.5 4.0 collective-permute-done.29
  563.5 6.0 collective-permute-done.28
  575.5 1.9 add_convert_fusion.3
  577.5 2.1 collective-permute-done.32
  584.3 2.5 collective-permute-start.34
  587.8 2.1 collective-permute-done.34
  591.4 2.9 collective-permute-done.35
  594.4 1.9 maximum_convert_fusion
  599.0 6.9 %collective-permute-done.30 = bf16[256,2048]{1,0:T(8,128)(2,1)S(1)} collective-permute-done((bf16[256,2048]{1,0:T(8,128)(2,1)}, bf16[256,2048]{1,0:T(8,128)(2,1)S(1)}, u32[]{:S(2)}, u32[]{:S(2)}) %collective-permute-start.30) | collective-permute-done | bytes 1048608 | tf_op jit(solution)/shard_map/ppermute | solution.py:542
  606.0 5.1 collective-permute-done.31
  611.1 3.3 convert_add_fusion
  614.4 1.9 copy.70
  618.3 2.9 copy.72
  621.2 2.4 fusion.11
  631.1 3.0 collective-permute-done.39
  634.2 2.7 collective-permute-done.38
  (383 shorter events, 124.9 us)
Async XLA Ops:
  7.2 108.8 %all-gather.5.cloned.1.call-start = ((), (), s32[]{:S(2)}) async-start(), calls=%async_computation.4 | async-start | bytes 2359296 | tf_op jit(solution)/shard_map/all_gather | solution.py:734
  7.9 118.0 %all-gather.7.cloned.1.call-start = ((), (), s32[]{:S(2)}) async-start(), calls=%async_computation.5 | async-start | bytes 9437184 | tf_op jit(solution)/shard_map/all_gather | solution.py:738
  15.4 11.1 %collective-permute-start.11 = (bf16[64,2048]{1,0:T(8,128)(2,1)S(1)}, bf16[64,2048]{1,0:T(8,128)(2,1)S(1)}, u32[]{:S(2)}, u32[]{:S(2)}) collective-permute-start(bf16[64,2048]{1,0:T(8,128)(2,1)S(1)} %bitcast.238), channel_id=1, source_target_pairs={{0,24},{8,16},{16,8},{24,0},{1,25},{9,17},{17,9},{25,1},{2,26},{10... | collective-permute-start | bytes 786440 | tf_op jit(solution)/shard_map/ppermute | solution.py:542
  19.5 11.8 %collective-permute-start.10 = (bf16[64,2048]{1,0:T(8,128)(2,1)S(1)}, bf16[64,2048]{1,0:T(8,128)(2,1)S(1)}, u32[]{:S(2)}, u32[]{:S(2)}) collective-permute-start(bf16[64,2048]{1,0:T(8,128)(2,1)S(1)} %bitcast.239), channel_id=1, source_target_pairs={{0,16},{8,24},{16,0},{24,8},{1,17},{9,25},{17,1},{25,9},{2,18},{10... | collective-permute-start | bytes 786440 | tf_op jit(solution)/shard_map/ppermute | solution.py:542
  20.2 11.3 %collective-permute-start.9 = (bf16[64,2048]{1,0:T(8,128)(2,1)S(1)}, bf16[64,2048]{1,0:T(8,128)(2,1)S(1)}, u32[]{:S(2)}, u32[]{:S(2)}) collective-permute-start(bf16[64,2048]{1,0:T(8,128)(2,1)S(1)} %bitcast.240), channel_id=1, source_target_pairs={{0,8},{8,0},{16,24},{24,16},{1,9},{9,1},{17,25},{25,17},{2,10},{10... | collective-permute-start | bytes 786440 | tf_op jit(solution)/shard_map/ppermute | solution.py:542
  33.0 233.9 %all-gather.9.cloned.1.call-start = ((), (), s32[]{:S(2)}) async-start(), calls=%async_computation.6 | async-start | bytes 12976128 | tf_op jit(solution)/shard_map/all_gather | solution.py:740
  37.2 12.3 %collective-permute-start.18 = (bf16[64,2816]{1,0:T(8,128)(2,1)S(1)}, bf16[64,2816]{1,0:T(8,128)(2,1)S(1)}, u32[]{:S(2)}, u32[]{:S(2)}) collective-permute-start(bf16[64,2816]{1,0:T(8,128)(2,1)S(1)} %bitcast.227), channel_id=1, source_target_pairs={{0,24},{8,16},{16,8},{24,0},{1,25},{9,17},{17,9},{25,1},{2,26},{10... | collective-permute-start | bytes 1081352 | tf_op jit(solution)/shard_map/ppermute | solution.py:542
  39.1 17.0 %collective-permute-start.17 = (bf16[64,2816]{1,0:T(8,128)(2,1)S(1)}, bf16[64,2816]{1,0:T(8,128)(2,1)S(1)}, u32[]{:S(2)}, u32[]{:S(2)}) collective-permute-start(bf16[64,2816]{1,0:T(8,128)(2,1)S(1)} %bitcast.228), channel_id=1, source_target_pairs={{0,16},{8,24},{16,0},{24,8},{1,17},{9,25},{17,1},{25,9},{2,18},{10... | collective-permute-start | bytes 1081352 | tf_op jit(solution)/shard_map/ppermute | solution.py:542
  40.4 16.0 %collective-permute-start.16 = (bf16[64,2816]{1,0:T(8,128)(2,1)S(1)}, bf16[64,2816]{1,0:T(8,128)(2,1)S(1)}, u32[]{:S(2)}, u32[]{:S(2)}) collective-permute-start(bf16[64,2816]{1,0:T(8,128)(2,1)S(1)} %bitcast.229), channel_id=1, source_target_pairs={{0,8},{8,0},{16,24},{24,16},{1,9},{9,1},{17,25},{25,17},{2,10},{10... | collective-permute-start | bytes 1081352 | tf_op jit(solution)/shard_map/ppermute | solution.py:542
  56.8 16.0 %copy-start.2 = (bf16[1,256,2048]{2,1,0:T(8,128)(2,1)S(1)}, bf16[1,256,2048]{2,1,0:T(8,128)(2,1)}, u32[]{:S(2)}) copy-start(bf16[1,256,2048]{2,1,0:T(8,128)(2,1)} %param.17) | copy-start | bytes 3145732
  58.1 241.2 %all-gather.11.cloned.1.call-start = ((), (), s32[]{:S(2)}) async-start(), calls=%async_computation.7 | async-start | bytes 6488064 | tf_op jit(solution)/shard_map/all_gather | solution.py:741
  58.9 1.2 collective-permute-start.4
  60.1 3.8 collective-permute-start.5
  64.0 7.1 %collective-permute-start.6 = (bf16[4,1608]{1,0:T(4,128)(2,1)S(1)}, bf16[4,1608]{1,0:T(4,128)(2,1)S(1)}, u32[]{:S(2)}, u32[]{:S(2)}) collective-permute-start(bf16[4,1608]{1,0:T(4,128)(2,1)S(1)} %pad_maximum_fusion.28), channel_id=1, source_target_pairs={{0,4},{1,5},{2,6},{3,7},{4,0},{5,1},{6,2},{7,3},{8,12},{9,13},{10,... | collective-permute-start | bytes 38600 | tf_op jit(solution)/shard_map/ppermute | solution.py:580
  71.2 6.8 %collective-permute-start.7 = (bf16[8,1608]{1,0:T(8,128)(2,1)S(1)}, bf16[8,1608]{1,0:T(8,128)(2,1)S(1)}, u32[]{:S(2)}, u32[]{:S(2)}) collective-permute-start(bf16[8,1608]{1,0:T(8,128)(2,1)S(1)} %pad_maximum_fusion.27), channel_id=1, source_target_pairs={{0,8},{8,0},{16,24},{24,16},{1,9},{9,1},{17,25},{25,17},{2,10},{10... | collective-permute-start | bytes 77192 | tf_op jit(solution)/shard_map/ppermute | solution.py:580
  75.9 28.9 %collective-permute-start = (bf16[256,2048]{1,0:T(8,128)(2,1)S(1)}, bf16[256,2048]{1,0:T(8,128)(2,1)}, u32[]{:S(2)}, u32[]{:S(2)}) collective-permute-start(bf16[256,2048]{1,0:T(8,128)(2,1)S(1)} %copy.61), channel_id=1, source_target_pairs={{0,8},{8,0},{16,24},{24,16},{1,9},{9,1},{17,25},{25,17},{2,10},{10... | collective-permute-start | bytes 3145736 | tf_op jit(solution)/shard_map/ppermute | solution.py:542
  76.5 23.7 %collective-permute-start.1 = (bf16[256,2048]{1,0:T(8,128)(2,1)S(1)}, bf16[256,2048]{1,0:T(8,128)(2,1)}, u32[]{:S(2)}, u32[]{:S(2)}) collective-permute-start(bf16[256,2048]{1,0:T(8,128)(2,1)S(1)} %copy.61), channel_id=1, source_target_pairs={{0,16},{8,24},{16,0},{24,8},{1,17},{9,25},{17,1},{25,9},{2,18},{10... | collective-permute-start | bytes 3145736 | tf_op jit(solution)/shard_map/ppermute | solution.py:542
  78.0 20.7 %collective-permute-start.8 = (bf16[16,1608]{1,0:T(8,128)(2,1)S(1)}, bf16[16,1608]{1,0:T(8,128)(2,1)S(1)}, u32[]{:S(2)}, u32[]{:S(2)}) collective-permute-start(bf16[16,1608]{1,0:T(8,128)(2,1)S(1)} %pad_maximum_fusion.26), channel_id=1, source_target_pairs={{0,16},{8,24},{16,0},{24,8},{1,17},{9,25},{17,1},{25,9},{2,18},{10... | collective-permute-start | bytes 154376 | tf_op jit(solution)/shard_map/ppermute | solution.py:580
  102.1 9.5 %collective-permute-start.2 = (bf16[128,2048]{1,0:T(8,128)(2,1)}, bf16[128,2048]{1,0:T(8,128)(2,1)}, u32[]{:S(2)}, u32[]{:S(2)}) collective-permute-start(bf16[128,2048]{1,0:T(8,128)(2,1)} %slice.292), channel_id=1, source_target_pairs={{0,8},{8,0},{16,24},{24,16},{1,9},{9,1},{17,25},{25,17},{2,10},{10... | collective-permute-start | bytes 1572872 | tf_op jit(solution)/shard_map/ppermute | solution.py:542
  104.4 16.4 %copy-start.43 = (bf16[16,2048]{1,0:T(8,128)(2,1)}, bf16[16,2048]{1,0:T(8,128)(2,1)S(1)}, u32[]{:S(2)}) copy-start(bf16[16,2048]{1,0:T(8,128)(2,1)S(1)} %reshape.368) | copy-start | bytes 196612
  104.5 19.4 %copy-start.52 = (bf16[256,16]{1,0:T(8,128)(2,1)}, bf16[256,16]{1,0:T(8,128)(2,1)S(1)}, u32[]{:S(2)}) copy-start(bf16[256,16]{1,0:T(8,128)(2,1)S(1)} %reshape.365) | copy-start | bytes 24580
  104.7 262.7 %reduce-scatter.5.cloned.1.call-start = ((), (), s32[]{:S(2)}) async-start(), calls=%async_computation.8 | async-start | bytes 6488064 | tf_op jit(solution)/shard_map/reduce_scatter | solution.py:833
  105.9 9.2 %collective-permute-start.3 = (bf16[128,2048]{1,0:T(8,128)(2,1)S(1)}, bf16[128,2048]{1,0:T(8,128)(2,1)S(1)}, u32[]{:S(2)}, u32[]{:S(2)}) collective-permute-start(bf16[128,2048]{1,0:T(8,128)(2,1)S(1)} %slice.293), channel_id=1, source_target_pairs={{0,16},{8,24},{16,0},{24,8},{1,17},{9,25},{17,1},{25,9},{2,18},{10... | collective-permute-start | bytes 1572872 | tf_op jit(solution)/shard_map/ppermute | solution.py:542
  124.0 17.2 %copy-start.51 = (bf16[1024,16]{0,1:T(8,128)(2,1)}, bf16[1024,16]{0,1:T(8,128)(2,1)S(1)}, u32[]{:S(2)}) copy-start(bf16[1024,16]{0,1:T(8,128)(2,1)S(1)} %convolution_convert_fusion.8) | copy-start | bytes 98308
  125.9 15.4 %copy-start.6 = (f32[128,1024]{1,0:T(8,128)S(1)}, f32[128,1024]{1,0:T(8,128)}, u32[]{:S(2)}) copy-start(f32[128,1024]{1,0:T(8,128)} %pad_maximum_fusion.22.rate) | copy-start | bytes 1572868
  125.9 34.3 %collective-permute-start.12 = (bf16[256,2048]{1,0:T(8,128)(2,1)}, bf16[256,2048]{1,0:T(8,128)(2,1)S(1)}, u32[]{:S(2)}, u32[]{:S(2)}) collective-permute-start(bf16[256,2048]{1,0:T(8,128)(2,1)} %bitcast.18.refs_1_), channel_id=1, source_target_pairs={{0,8},{8,0},{16,24},{24,16},{1,9},{9,1},{17,25},{25,17},{2,10},{10... | collective-permute-start | bytes 3145736 | tf_op jit(solution)/shard_map/ppermute | solution.py:542
  127.3 30.8 %collective-permute-start.13 = (bf16[256,2048]{1,0:T(8,128)(2,1)}, bf16[256,2048]{1,0:T(8,128)(2,1)S(1)}, u32[]{:S(2)}, u32[]{:S(2)}) collective-permute-start(bf16[256,2048]{1,0:T(8,128)(2,1)} %bitcast.18.refs_1_), channel_id=1, source_target_pairs={{0,16},{8,24},{16,0},{24,8},{1,17},{9,25},{17,1},{25,9},{2,18},{10... | collective-permute-start | bytes 3145736 | tf_op jit(solution)/shard_map/ppermute | solution.py:542
  141.2 12.0 %copy-start = (bf16[1024,2048]{1,0:T(8,128)(2,1)}, bf16[1024,2048]{1,0:T(8,128)(2,1)S(1)}, u32[]{:S(2)}) copy-start(bf16[1024,2048]{1,0:T(8,128)(2,1)S(1)} %get-tuple-element.247.query.key.value) | copy-start | bytes 12582916
  141.2 12.2 %copy-start.31 = (f32[1024,2048]{1,0:T(8,128)}, f32[1024,2048]{1,0:T(8,128)S(1)}, u32[]{:S(2)}) copy-start(f32[1024,2048]{1,0:T(8,128)S(1)} %get-tuple-element.248) | copy-start | bytes 25165828
  158.2 13.6 %collective-permute-start.14 = (bf16[128,2048]{1,0:T(8,128)(2,1)S(1)}, bf16[128,2048]{1,0:T(8,128)(2,1)S(1)}, u32[]{:S(2)}, u32[]{:S(2)}) collective-permute-start(bf16[128,2048]{1,0:T(8,128)(2,1)S(1)} %slice.296), channel_id=1, source_target_pairs={{0,8},{8,0},{16,24},{24,16},{1,9},{9,1},{17,25},{25,17},{2,10},{10... | collective-permute-start | bytes 1572872 | tf_op jit(solution)/shard_map/ppermute | solution.py:542
  160.2 13.3 %collective-permute-start.15 = (bf16[128,2048]{1,0:T(8,128)(2,1)S(1)}, bf16[128,2048]{1,0:T(8,128)(2,1)S(1)}, u32[]{:S(2)}, u32[]{:S(2)}) collective-permute-start(bf16[128,2048]{1,0:T(8,128)(2,1)S(1)} %slice.297), channel_id=1, source_target_pairs={{0,16},{8,24},{16,0},{24,8},{1,17},{9,25},{17,1},{25,9},{2,18},{10... | collective-permute-start | bytes 1572872 | tf_op jit(solution)/shard_map/ppermute | solution.py:542
  299.3 173.3 %reduce-scatter.7.cloned.1.call-start = ((), (), s32[]{:S(2)}) async-start(), calls=%async_computation.9 | async-start | bytes 7208960 | tf_op jit(solution)/shard_map/reduce_scatter | solution.py:633
  316.3 17.8 %copy-start.10 = (bf16[4,256,2048]{2,1,0:T(8,128)(2,1)S(1)}, bf16[4,256,2048]{2,1,0:T(8,128)(2,1)}, u32[]{:S(2)}) copy-start(bf16[4,256,2048]{2,1,0:T(8,128)(2,1)} %copy-done.9) | copy-start | bytes 12582916
  345.9 12.9 %collective-permute-start.19 = (bf16[1024,2816]{1,0:T(8,128)(2,1)}, bf16[1024,2816]{1,0:T(8,128)(2,1)S(1)}, u32[]{:S(2)}, u32[]{:S(2)}) collective-permute-start(bf16[1024,2816]{1,0:T(8,128)(2,1)} %convolution_convert_fusion.2), channel_id=1, source_target_pairs={{0,1},{1,0},{2,3},{3,2},{4,5},{5,4},{6,7},{7,6},{8,9},{9,8},{10,11... | collective-permute-start | bytes 17301512 | tf_op jit(solution)/shard_map/ppermute | solution.py:580
  367.5 143.6 %reduce-scatter.9.cloned.1.call-start = ((), (), s32[]{:S(2)}) async-start(), calls=%async_computation.10 | async-start | bytes 1310720 | tf_op jit(solution)/shard_map/reduce_scatter | solution.py:633
  371.5 76.8 %copy-start.28 = (bf16[1024,2048]{1,0:T(8,128)(2,1)S(1)}, bf16[1024,2048]{1,0:T(8,128)(2,1)}, u32[]{:S(2)}) copy-start(bf16[1024,2048]{1,0:T(8,128)(2,1)} %convolution_convert_fusion.4) | copy-start | bytes 12582916
  448.5 13.4 %collective-permute-start.20 = (bf16[128,2048]{1,0:T(8,128)(2,1)S(1)}, bf16[128,2048]{1,0:T(8,128)(2,1)S(1)}, u32[]{:S(2)}, u32[]{:S(2)}) collective-permute-start(bf16[128,2048]{1,0:T(8,128)(2,1)S(1)} %get-tuple-element.149), channel_id=1, source_target_pairs={{0,8},{8,0},{16,24},{24,16},{1,9},{9,1},{17,25},{25,17},{2,10},{10... | collective-permute-start | bytes 1572872 | tf_op jit(solution)/shard_map/ppermute | solution.py:542
  450.1 13.3 %collective-permute-start.21 = (bf16[128,2048]{1,0:T(8,128)(2,1)S(1)}, bf16[128,2048]{1,0:T(8,128)(2,1)S(1)}, u32[]{:S(2)}, u32[]{:S(2)}) collective-permute-start(bf16[128,2048]{1,0:T(8,128)(2,1)S(1)} %get-tuple-element.148), channel_id=1, source_target_pairs={{0,16},{8,24},{16,0},{24,8},{1,17},{9,25},{17,1},{25,9},{2,18},{10... | collective-permute-start | bytes 1572872 | tf_op jit(solution)/shard_map/ppermute | solution.py:542
  466.4 4.7 collective-permute-start.24
  468.0 30.0 %collective-permute-start.22 = (bf16[256,2048]{1,0:T(8,128)(2,1)}, bf16[256,2048]{1,0:T(8,128)(2,1)}, u32[]{:S(2)}, u32[]{:S(2)}) collective-permute-start(bf16[256,2048]{1,0:T(8,128)(2,1)} %pad_maximum_fusion.15), channel_id=1, source_target_pairs={{0,8},{8,0},{16,24},{24,16},{1,9},{9,1},{17,25},{25,17},{2,10},{10... | collective-permute-start | bytes 3145736 | tf_op jit(solution)/shard_map/ppermute | solution.py:542
  469.4 28.5 %collective-permute-start.23 = (bf16[256,2048]{1,0:T(8,128)(2,1)}, bf16[256,2048]{1,0:T(8,128)(2,1)}, u32[]{:S(2)}, u32[]{:S(2)}) collective-permute-start(bf16[256,2048]{1,0:T(8,128)(2,1)} %pad_maximum_fusion.16), channel_id=1, source_target_pairs={{0,16},{8,24},{16,0},{24,8},{1,17},{9,25},{17,1},{25,9},{2,18},{10... | collective-permute-start | bytes 3145736 | tf_op jit(solution)/shard_map/ppermute | solution.py:542
  472.6 151.0 %reduce-scatter.11.cloned.1.call-start = ((), (), s32[]{:S(2)}) async-start(), calls=%async_computation.11 | async-start | bytes 9437184 | tf_op jit(solution)/shard_map/reduce_scatter | solution.py:889
  476.7 22.9 %copy-start.20 = (bf16[1024,2048]{1,0:T(8,128)(2,1)S(1)}, bf16[1024,2048]{1,0:T(8,128)(2,1)}, u32[]{:S(2)}) copy-start(bf16[1024,2048]{1,0:T(8,128)(2,1)} %copy-done.19) | copy-start | bytes 12582916
  476.7 22.9 %copy-start.38 = (bf16[1024,512]{1,0:T(8,128)(2,1)S(1)}, bf16[1024,512]{1,0:T(8,128)(2,1)}, u32[]{:S(2)}) copy-start(bf16[1024,512]{1,0:T(8,128)(2,1)} %get-tuple-element.136) | copy-start | bytes 3145732
  519.0 12.4 %copy-start.34 = (bf16[64,1024]{1,0:T(8,128)(2,1)}, bf16[64,1024]{1,0:T(8,128)(2,1)S(1)}, u32[]{:S(2)}) copy-start(bf16[64,1024]{1,0:T(8,128)(2,1)S(1)} %get-tuple-element.133) | copy-start | bytes 393220
  519.9 11.5 %copy-start.44 = (bf16[16,2048]{1,0:T(8,128)(2,1)S(1)}, bf16[16,2048]{1,0:T(8,128)(2,1)}, u32[]{:S(2)}) copy-start(bf16[16,2048]{1,0:T(8,128)(2,1)} %copy-done.43) | copy-start | bytes 196612
  519.9 11.5 %copy-start.54 = (f32[1024]{0:T(1024)S(1)}, f32[1024]{0:T(1024)}, u32[]{:S(2)}) copy-start(f32[1024]{0:T(1024)} %copy-done.53) | copy-start | bytes 12292
  536.6 33.4 %collective-permute-start.25 = (bf16[128,2048]{1,0:T(8,128)(2,1)}, bf16[128,2048]{1,0:T(8,128)(2,1)}, u32[]{:S(2)}, u32[]{:S(2)}) collective-permute-start(bf16[128,2048]{1,0:T(8,128)(2,1)} %get-tuple-element.143), channel_id=1, source_target_pairs={{0,8},{8,0},{16,24},{24,16},{1,9},{9,1},{17,25},{25,17},{2,10},{10... | collective-permute-start | bytes 1572872 | tf_op jit(solution)/shard_map/ppermute | solution.py:542
  536.8 33.3 %collective-permute-start.26 = (bf16[128,2048]{1,0:T(8,128)(2,1)}, bf16[128,2048]{1,0:T(8,128)(2,1)}, u32[]{:S(2)}, u32[]{:S(2)}) collective-permute-start(bf16[128,2048]{1,0:T(8,128)(2,1)} %get-tuple-element.142), channel_id=1, source_target_pairs={{0,16},{8,24},{16,0},{24,8},{1,17},{9,25},{17,1},{25,9},{2,18},{10... | collective-permute-start | bytes 1572872 | tf_op jit(solution)/shard_map/ppermute | solution.py:542
  542.8 12.0 %copy-start.5 = (f32[256,2048]{1,0:T(8,128)S(1)}, f32[256,2048]{1,0:T(8,128)}, u32[]{:S(2)}) copy-start(f32[256,2048]{1,0:T(8,128)} %copy-done.3) | copy-start | bytes 6291460
  551.2 12.4 %collective-permute-start.29 = (bf16[64,2816]{1,0:T(8,128)(2,1)S(1)}, bf16[64,2816]{1,0:T(8,128)(2,1)S(1)}, u32[]{:S(2)}, u32[]{:S(2)}) collective-permute-start(bf16[64,2816]{1,0:T(8,128)(2,1)S(1)} %get-tuple-element.180), channel_id=1, source_target_pairs={{0,24},{8,16},{16,8},{24,0},{1,25},{9,17},{17,9},{25,1},{2,26},{10... | collective-permute-start | bytes 1081352 | tf_op jit(solution)/shard_map/ppermute | solution.py:542
  553.0 16.6 %collective-permute-start.28 = (bf16[64,2816]{1,0:T(8,128)(2,1)S(1)}, bf16[64,2816]{1,0:T(8,128)(2,1)S(1)}, u32[]{:S(2)}, u32[]{:S(2)}) collective-permute-start(bf16[64,2816]{1,0:T(8,128)(2,1)S(1)} %get-tuple-element.181), channel_id=1, source_target_pairs={{0,16},{8,24},{16,0},{24,8},{1,17},{9,25},{17,1},{25,9},{2,18},{10... | collective-permute-start | bytes 1081352 | tf_op jit(solution)/shard_map/ppermute | solution.py:542
  553.1 16.4 %collective-permute-start.27 = (bf16[64,2816]{1,0:T(8,128)(2,1)S(1)}, bf16[64,2816]{1,0:T(8,128)(2,1)S(1)}, u32[]{:S(2)}, u32[]{:S(2)}) collective-permute-start(bf16[64,2816]{1,0:T(8,128)(2,1)S(1)} %get-tuple-element.182), channel_id=1, source_target_pairs={{0,8},{8,0},{16,24},{24,16},{1,9},{9,1},{17,25},{25,17},{2,10},{10... | collective-permute-start | bytes 1081352 | tf_op jit(solution)/shard_map/ppermute | solution.py:542
  574.9 11.9 %copy-start.32 = (bf16[128,2048]{1,0:T(8,128)(2,1)S(1)}, bf16[128,2048]{1,0:T(8,128)(2,1)}, u32[]{:S(2)}) copy-start(bf16[128,2048]{1,0:T(8,128)(2,1)} %get-tuple-element.141) | copy-start | bytes 1572868
  574.9 4.7 collective-permute-start.32
  579.6 4.6 collective-permute-start.33
  581.3 24.7 %collective-permute-start.30 = (bf16[256,2048]{1,0:T(8,128)(2,1)}, bf16[256,2048]{1,0:T(8,128)(2,1)S(1)}, u32[]{:S(2)}, u32[]{:S(2)}) collective-permute-start(bf16[256,2048]{1,0:T(8,128)(2,1)} %pad_maximum_fusion.19), channel_id=1, source_target_pairs={{0,8},{8,0},{16,24},{24,16},{1,9},{9,1},{17,25},{25,17},{2,10},{10... | collective-permute-start | bytes 3145736 | tf_op jit(solution)/shard_map/ppermute | solution.py:542
  584.3 5.7 collective-permute-start.34
  587.8 23.3 %collective-permute-start.31 = (bf16[256,2048]{1,0:T(8,128)(2,1)}, bf16[256,2048]{1,0:T(8,128)(2,1)}, u32[]{:S(2)}, u32[]{:S(2)}) collective-permute-start(bf16[256,2048]{1,0:T(8,128)(2,1)} %pad_maximum_fusion.20), channel_id=1, source_target_pairs={{0,16},{8,24},{16,0},{24,8},{1,17},{9,25},{17,1},{25,9},{2,18},{10... | collective-permute-start | bytes 3145736 | tf_op jit(solution)/shard_map/ppermute | solution.py:542
  590.0 4.3 collective-permute-start.35
  594.3 2.0 collective-permute-start.36
  625.1 9.1 %collective-permute-start.39 = (bf16[64,2048]{1,0:T(8,128)(2,1)S(1)}, bf16[64,2048]{1,0:T(8,128)(2,1)S(1)}, u32[]{:S(2)}, u32[]{:S(2)}) collective-permute-start(bf16[64,2048]{1,0:T(8,128)(2,1)S(1)} %get-tuple-element.208), channel_id=1, source_target_pairs={{0,24},{8,16},{16,8},{24,0},{1,25},{9,17},{17,9},{25,1},{2,26},{10... | collective-permute-start | bytes 786440 | tf_op jit(solution)/shard_map/ppermute | solution.py:542
  626.6 10.2 %collective-permute-start.38 = (bf16[64,2048]{1,0:T(8,128)(2,1)S(1)}, bf16[64,2048]{1,0:T(8,128)(2,1)S(1)}, u32[]{:S(2)}, u32[]{:S(2)}) collective-permute-start(bf16[64,2048]{1,0:T(8,128)(2,1)S(1)} %get-tuple-element.209), channel_id=1, source_target_pairs={{0,16},{8,24},{16,0},{24,8},{1,17},{9,25},{17,1},{25,9},{2,18},{10... | collective-permute-start | bytes 786440 | tf_op jit(solution)/shard_map/ppermute | solution.py:542
  626.9 9.9 %collective-permute-start.37 = (bf16[64,2048]{1,0:T(8,128)(2,1)S(1)}, bf16[64,2048]{1,0:T(8,128)(2,1)S(1)}, u32[]{:S(2)}, u32[]{:S(2)}) collective-permute-start(bf16[64,2048]{1,0:T(8,128)(2,1)S(1)} %get-tuple-element.210), channel_id=1, source_target_pairs={{0,8},{8,0},{16,24},{24,16},{1,9},{9,1},{17,25},{25,17},{2,10},{10... | collective-permute-start | bytes 786440 | tf_op jit(solution)/shard_map/ppermute | solution.py:542
  (55 other events, 204.6 us)
Sparse Core Ops, SparseCore 0:
  9.6 31.7 all-gather.4
  43.6 82.1 all-gather.6
  128.0 106.4 all-gather.8
  236.0 58.7 all-gather.10
  299.4 64.9 reduce-scatter.4
  367.6 102.3 reduce-scatter.6
  472.8 27.6 reduce-scatter.8
  511.2 90.3 reduce-scatter.10
